TPU v7x, 8 devices: a whole 2x2x1 slice. The times are simulated.
8 devices in a mesh: model: 4 (over z, y, x), data: 2 (over core).
Axes of the slice: x: 2, y: 2, z: 1, core: 2. Of those that a mesh axis runs over, the one named last changes fastest.
Arguments:
- x_in: bfloat16 [4, 1024, 1536], P('data')
- cot_out: bfloat16 [4, 1024, 1536], P('data')
- step_emb: bfloat16 [4, 1536], replicated
- w_q: bfloat16 [1536, 1536], P(None, 'model')
- w_k: bfloat16 [1536, 1536], P(None, 'model')
- w_v: bfloat16 [1536, 1536], P(None, 'model')
- w_o: bfloat16 [1536, 1536], P('model')
- w_1: bfloat16 [1536, 6144], P(None, 'model')
- w_2: bfloat16 [6144, 1536], P('model')
Outputs:
- output 1: float32 [1536, 1536], P(None, 'model')
- output 2: float32 [1536, 1536], P(None, 'model')
- output 3: float32 [1536, 1536], P(None, 'model')
- output 4: float32 [1536, 1536], P('model')
- output 5: float32 [1536, 6144], P(None, 'model')
- output 6: float32 [6144, 1536], P('model')
- output 7: bfloat16 [4, 1024, 1536], P('data')
All inputs are finite; a program needn't handle non-finite values.
Results may differ from a plain program's by a relative error of at most 0.0181743.
Values are sent between devices in bfloat16 or wider.
A program may use at most 1 GiB of HBM per device.

v0:
```python
import jax
import jax.numpy as jnp
from jax import lax
from jax.sharding import PartitionSpec as P

HEAD_DIM = 64
EPS_NORM = 1e-6


def rms_norm(values):
    return values * lax.rsqrt(jnp.mean(values * values, axis=-1, keepdims=True) + EPS_NORM)


def split_heads(qkv):
    batch_size, seq_len, triple_width = qkv.shape
    stacked = qkv.reshape(batch_size, seq_len, 3, triple_width // (3 * HEAD_DIM), HEAD_DIM)
    return stacked[:, :, 0], stacked[:, :, 1], stacked[:, :, 2]


def attn_probs(q_head, k_head):
    scores = jnp.einsum('bqhe,bkhe->bhqk', q_head, k_head, preferred_element_type=jnp.float32)
    return jax.nn.softmax(scores * (HEAD_DIM ** -0.5), axis=-1)


def layer_forward(x_cur, step_vec, w_qkv, w_out, w_up, w_down, reduce_model):
    batch_size, seq_len = x_cur.shape[0], x_cur.shape[1]
    x_f = x_cur.astype(jnp.float32) + step_vec.astype(jnp.float32)
    u_in = rms_norm(x_f).astype(jnp.bfloat16)
    qkv = jnp.einsum('bsd,de->bse', u_in, w_qkv, preferred_element_type=jnp.float32).astype(jnp.bfloat16)
    q_head, k_head, v_head = split_heads(qkv)
    prob_mat = attn_probs(q_head, k_head).astype(jnp.bfloat16)
    context = jnp.einsum('bhqk,bkhe->bqhe', prob_mat, v_head, preferred_element_type=jnp.float32)
    context = context.astype(jnp.bfloat16).reshape(batch_size, seq_len, w_out.shape[0])
    attn_out = reduce_model(jnp.einsum('bse,ed->bsd', context, w_out, preferred_element_type=jnp.float32))
    h_mid = (x_f + attn_out).astype(jnp.bfloat16)
    m_in = rms_norm(h_mid.astype(jnp.float32)).astype(jnp.bfloat16)
    z_up = jnp.einsum('bsd,df->bsf', m_in, w_up, preferred_element_type=jnp.float32).astype(jnp.bfloat16)
    g_act = jax.nn.gelu(z_up.astype(jnp.float32)).astype(jnp.bfloat16)
    mlp_out = reduce_model(jnp.einsum('bsf,fd->bsd', g_act, w_down, preferred_element_type=jnp.float32))
    x_next = (h_mid.astype(jnp.float32) + mlp_out).astype(jnp.bfloat16)
    return x_next, (x_cur, u_in, qkv, context, h_mid, m_in, z_up, g_act)


def layer_backward(d_next, step_vec, saved_acts, w_qkv, w_out, w_up, w_down, reduce_model):
    x_cur, u_in, qkv, context, h_mid, m_in, z_up, g_act = saved_acts
    batch_size, seq_len = x_cur.shape[0], x_cur.shape[1]
    grad_down = jnp.einsum('bsf,bsd->fd', g_act, d_next, preferred_element_type=jnp.float32)
    d_act = jnp.einsum('bsd,fd->bsf', d_next, w_down, preferred_element_type=jnp.float32).astype(jnp.bfloat16)
    gelu_pull = jax.vjp(jax.nn.gelu, z_up.astype(jnp.float32))[1]
    d_up = gelu_pull(d_act.astype(jnp.float32))[0].astype(jnp.bfloat16)
    grad_up = jnp.einsum('bsd,bsf->df', m_in, d_up, preferred_element_type=jnp.float32)
    d_norm2 = reduce_model(jnp.einsum('bsf,df->bsd', d_up, w_up, preferred_element_type=jnp.float32)).astype(jnp.bfloat16)
    norm_pull = jax.vjp(rms_norm, h_mid.astype(jnp.float32))[1]
    d_mid = (d_next.astype(jnp.float32) + norm_pull(d_norm2.astype(jnp.float32))[0]).astype(jnp.bfloat16)
    grad_wo = jnp.einsum('bse,bsd->ed', context, d_mid, preferred_element_type=jnp.float32)
    head_shape = (batch_size, seq_len, w_out.shape[0] // HEAD_DIM, HEAD_DIM)
    d_context = jnp.einsum('bsd,ed->bse', d_mid, w_out, preferred_element_type=jnp.float32).astype(jnp.bfloat16).reshape(head_shape)
    q_head, k_head, v_head = split_heads(qkv)
    prob_f = attn_probs(q_head, k_head)
    d_prob = jnp.einsum('bqhe,bkhe->bhqk', d_context, v_head, preferred_element_type=jnp.float32).astype(jnp.bfloat16).astype(jnp.float32)
    d_value = jnp.einsum('bhqk,bqhe->bkhe', prob_f.astype(jnp.bfloat16), d_context, preferred_element_type=jnp.float32).astype(jnp.bfloat16)
    d_scores = (prob_f * (d_prob - jnp.sum(prob_f * d_prob, axis=-1, keepdims=True)) * (HEAD_DIM ** -0.5)).astype(jnp.bfloat16)
    d_query = jnp.einsum('bhqk,bkhe->bqhe', d_scores, k_head, preferred_element_type=jnp.float32).astype(jnp.bfloat16)
    d_key = jnp.einsum('bhqk,bqhe->bkhe', d_scores, q_head, preferred_element_type=jnp.float32).astype(jnp.bfloat16)
    d_qkv = jnp.stack([d_query, d_key, d_value], axis=2).reshape(batch_size, seq_len, w_qkv.shape[1])
    grad_qkv = jnp.einsum('bsd,bse->de', u_in, d_qkv, preferred_element_type=jnp.float32)
    d_norm1 = reduce_model(jnp.einsum('bse,de->bsd', d_qkv, w_qkv, preferred_element_type=jnp.float32)).astype(jnp.bfloat16)
    x_f = x_cur.astype(jnp.float32) + step_vec.astype(jnp.float32)
    norm_pull_x = jax.vjp(rms_norm, x_f)[1]
    d_prev = (d_mid.astype(jnp.float32) + norm_pull_x(d_norm1.astype(jnp.float32))[0]).astype(jnp.bfloat16)
    return d_prev, (grad_qkv, grad_wo, grad_up, grad_down)


def solution(mesh):
    spec_col = P(None, 'model')
    spec_row = P('model', None)
    spec_act = P('data', None, None)
    spec_rep = P(None, None)

    def sum_model(values):
        return lax.psum(values, 'model')

    def device_step(x_in, cot_out, step_emb, w_q, w_k, w_v, w_o, w_1, w_2):
        w_qkv = jnp.concatenate([w_q, w_k, w_v], axis=1)
        layer_count = step_emb.shape[0]
        x_cur = x_in
        saved_list = []
        for layer_idx in range(layer_count):
            x_cur, saved_acts = layer_forward(x_cur, step_emb[layer_idx], w_qkv, w_o, w_1, w_2, sum_model)
            saved_list.append(saved_acts)
        d_cur = cot_out
        totals = None
        for layer_idx in reversed(range(layer_count)):
            d_cur, layer_grads = layer_backward(d_cur, step_emb[layer_idx], saved_list[layer_idx], w_qkv, w_o, w_1, w_2, sum_model)
            layer_grads = lax.psum(layer_grads, 'data')
            if totals is None:
                totals = layer_grads
            else:
                totals = jax.tree.map(jnp.add, totals, layer_grads)
        grad_qkv, grad_wo, grad_up, grad_down = totals
        col_width = w_q.shape[1]
        return (grad_qkv[:, :col_width], grad_qkv[:, col_width:2 * col_width], grad_qkv[:, 2 * col_width:],
                grad_wo, grad_up, grad_down, d_cur)

    return jax.shard_map(device_step, mesh=mesh,
                         in_specs=(spec_act, spec_act, spec_rep, spec_col, spec_col, spec_col, spec_row, spec_col, spec_row),
                         out_specs=(spec_col, spec_col, spec_col, spec_row, spec_col, spec_row, spec_act),
                         check_vma=False)
```

profile of v0, /device:TPU:0, one launch (start us, length us, event | category | flops | bytes accessed | tf_op | source)
XLA Modules:
  0.0 6458.1 jit_solution(9029033116063583046)
XLA Ops:
  34.1 23.6 fusion.328
  57.6 17.3 fusion.212
  82.6 230.6 %all-reduce.18.cloned.1.call-done = f32[2,1024,1536]{2,1,0:T(8,128)} async-done(((f32[2,1024,1536]{2,1,0:T(8,128)}), f32[2,1024,1536]{2,1,0:T(8,128)}) %all-reduce.18.cloned.1.call-update) | async-done | bytes 12582928 | tf_op jit(solution)/shard_map/psum | solution.py:81
  321.8 13.8 fusion.178
  338.3 13.8 fusion.195
  352.1 227.7 %all-reduce.20.cloned.1.call-done = f32[2,1024,1536]{2,1,0:T(8,128)} async-done(((f32[2,1024,1536]{2,1,0:T(8,128)}), f32[2,1024,1536]{2,1,0:T(8,128)}) %all-reduce.20.cloned.1.call-update) | async-done | bytes 12582928 | tf_op jit(solution)/shard_map/psum | solution.py:81
  607.8 22.9 fusion.329
  630.7 17.4 fusion.218
  655.6 227.8 %all-reduce.22.cloned.1.call-done = f32[2,1024,1536]{2,1,0:T(8,128)} async-done(((f32[2,1024,1536]{2,1,0:T(8,128)}), f32[2,1024,1536]{2,1,0:T(8,128)}) %all-reduce.22.cloned.1.call-update) | async-done | bytes 12582928 | tf_op jit(solution)/shard_map/psum | solution.py:81
  892.2 13.8 fusion.181
  908.8 13.8 fusion.193
  922.6 227.8 %all-reduce.24.cloned.1.call-done = f32[2,1024,1536]{2,1,0:T(8,128)} async-done(((f32[2,1024,1536]{2,1,0:T(8,128)}), f32[2,1024,1536]{2,1,0:T(8,128)}) %all-reduce.24.cloned.1.call-update) | async-done | bytes 12582928 | tf_op jit(solution)/shard_map/psum | solution.py:81
  1177.5 22.8 fusion.330
  1200.4 17.4 fusion.224
  1225.3 227.8 %all-reduce.26.cloned.1.call-done = f32[2,1024,1536]{2,1,0:T(8,128)} async-done(((f32[2,1024,1536]{2,1,0:T(8,128)}), f32[2,1024,1536]{2,1,0:T(8,128)}) %all-reduce.26.cloned.1.call-update) | async-done | bytes 12582928 | tf_op jit(solution)/shard_map/psum | solution.py:81
  1461.6 13.8 fusion.184
  1478.1 13.8 fusion.191
  1492.0 227.8 %all-reduce.28.cloned.1.call-done = f32[2,1024,1536]{2,1,0:T(8,128)} async-done(((f32[2,1024,1536]{2,1,0:T(8,128)}), f32[2,1024,1536]{2,1,0:T(8,128)}) %all-reduce.28.cloned.1.call-update) | async-done | bytes 12582928 | tf_op jit(solution)/shard_map/psum | solution.py:81
  1747.2 23.5 fusion.331
  1770.7 17.3 fusion.230
  1795.6 227.7 %all-reduce.30.cloned.1.call-done = f32[2,1024,1536]{2,1,0:T(8,128)} async-done(((f32[2,1024,1536]{2,1,0:T(8,128)}), f32[2,1024,1536]{2,1,0:T(8,128)}) %all-reduce.30.cloned.1.call-update) | async-done | bytes 12582928 | tf_op jit(solution)/shard_map/psum | solution.py:81
  2032.1 15.8 fusion.175
  2048.0 19.0 fusion.62
  2067.0 14.7 fusion.154
  2081.7 13.1 fusion.171
  2094.8 14.8 fusion.203
  2109.6 419.4 %all-reduce.33 = bf16[2,1024,1536]{2,1,0:T(8,128)(2,1)} all-reduce(f32[2,1024,1536]{2,1,0:T(8,128)} %fusion.203), channel_id=1, replica_groups=mesh['model'=4,'data'=2] {'model'}, use_global_device_ids=true, to_apply=%region_23.0 | all-reduce | flops 3145728 | bytes 18874368 | tf_op jit(solution)/shard_map/psum | solution.py:81
  2545.7 19.0 fusion.252
  2564.6 13.4 convolution_convert_fusion.3
  2578.0 49.6 fusion.245
  2627.6 49.8 fusion.244
  2704.5 415.5 %all-reduce.34 = bf16[2,1024,1536]{2,1,0:T(8,128)(2,1)} all-reduce(f32[2,1024,1536]{2,1,0:T(8,128)} %fusion.323), channel_id=1, replica_groups=mesh['model'=4,'data'=2] {'model'}, use_global_device_ids=true, to_apply=%region_27.0 | all-reduce | flops 3145728 | bytes 18874368 | tf_op jit(solution)/shard_map/psum | solution.py:81
  3134.3 23.0 fusion.66
  3157.4 14.5 fusion.312
  3171.9 13.5 fusion.160
  3198.0 414.7 %all-reduce.35 = bf16[2,1024,1536]{2,1,0:T(8,128)(2,1)} all-reduce(f32[2,1024,1536]{2,1,0:T(8,128)} %fusion.201), channel_id=1, replica_groups=mesh['model'=4,'data'=2] {'model'}, use_global_device_ids=true, to_apply=%region_29.0 | all-reduce | flops 3145728 | bytes 18874368 | tf_op jit(solution)/shard_map/psum | solution.py:81
  3633.4 18.9 fusion.255
  3652.4 13.3 convolution_convert_fusion.2
  3665.7 49.6 fusion.247
  3715.3 49.8 fusion.246
  3781.6 414.4 %all-reduce.36 = bf16[2,1024,1536]{2,1,0:T(8,128)(2,1)} all-reduce(f32[2,1024,1536]{2,1,0:T(8,128)} %fusion.322), channel_id=1, replica_groups=mesh['model'=4,'data'=2] {'model'}, use_global_device_ids=true, to_apply=%region_33.0 | all-reduce | flops 3145728 | bytes 18874368 | tf_op jit(solution)/shard_map/psum | solution.py:81
  4210.3 23.0 fusion.70
  4233.3 14.5 fusion.315
  4247.9 13.3 fusion.164
  4273.8 412.9 %all-reduce.37 = bf16[2,1024,1536]{2,1,0:T(8,128)(2,1)} all-reduce(f32[2,1024,1536]{2,1,0:T(8,128)} %fusion.199), channel_id=1, replica_groups=mesh['model'=4,'data'=2] {'model'}, use_global_device_ids=true, to_apply=%region_35.0 | all-reduce | flops 3145728 | bytes 18874368 | tf_op jit(solution)/shard_map/psum | solution.py:81
  4707.5 18.9 fusion.258
  4726.5 13.3 convolution_convert_fusion.1
  4739.8 49.9 fusion.249
  4789.6 49.8 fusion.248
  4856.0 412.4 %all-reduce.38 = bf16[2,1024,1536]{2,1,0:T(8,128)(2,1)} all-reduce(f32[2,1024,1536]{2,1,0:T(8,128)} %fusion.321), channel_id=1, replica_groups=mesh['model'=4,'data'=2] {'model'}, use_global_device_ids=true, to_apply=%region_39.0 | all-reduce | flops 3145728 | bytes 18874368 | tf_op jit(solution)/shard_map/psum | solution.py:81
  5282.6 22.4 fusion.74
  5307.6 14.6 fusion.197
  5322.2 411.4 %all-reduce.39 = bf16[2,1024,1536]{2,1,0:T(8,128)(2,1)} all-reduce(f32[2,1024,1536]{2,1,0:T(8,128)} %fusion.197), channel_id=1, replica_groups=mesh['model'=4,'data'=2] {'model'}, use_global_device_ids=true, to_apply=%region_41.0 | all-reduce | flops 3145728 | bytes 18874368 | tf_op jit(solution)/shard_map/psum | solution.py:81
  5750.2 19.0 fusion.261
  5769.1 13.4 convolution_convert_fusion
  5782.5 49.1 fusion.251
  5831.7 49.7 fusion.250
  5881.4 15.6 fusion.153
  5897.1 15.0 fusion.152
  5927.7 13.4 fusion.151
  5941.1 23.8 bitcast_add_fusion
  5964.9 22.4 bitcast_add_fusion.3
  5989.0 13.5 fusion.320
  6002.4 411.0 %all-reduce.40 = bf16[2,1024,1536]{2,1,0:T(8,128)(2,1)} all-reduce(f32[2,1024,1536]{2,1,0:T(8,128)} %fusion.320), channel_id=1, replica_groups=mesh['model'=4,'data'=2] {'model'}, use_global_device_ids=true, to_apply=%region_57.0 | all-reduce | flops 3145728 | bytes 18874368 | tf_op jit(solution)/shard_map/psum | solution.py:81
  (398 shorter events, 442.1 us)
Async XLA Ops:
  7.2 69.1 %copy-start = (bf16[384,1536]{1,0:T(8,128)(2,1)S(1)}, bf16[384,1536]{1,0:T(8,128)(2,1)}, u32[]{:S(2)}) copy-start(bf16[384,1536]{1,0:T(8,128)(2,1)} %param.15) | copy-start | bytes 3538948
  7.2 306.0 %all-reduce.18.cloned.1.call-start = ((), (), s32[]{:S(2)}) async-start(), calls=%async_computation | async-start | bytes 25165824 | tf_op jit(solution)/shard_map/psum | solution.py:81
  8.8 304.4 %copy-start.45 = (f32[1536]{0:T(1024)}, f32[1536]{0:T(1024)S(1)}, u32[]{:S(2)}) copy-start(f32[1536]{0:T(1024)S(1)} %get-tuple-element.9) | copy-start | bytes 18436
  8.8 874.6 %copy-start.47 = (f32[1536]{0:T(1024)}, f32[1536]{0:T(1024)S(1)}, u32[]{:S(2)}) copy-start(f32[1536]{0:T(1024)S(1)} %get-tuple-element.8) | copy-start | bytes 18436
  57.6 17.4 copy-start.111
  82.6 497.3 %all-reduce.20.cloned.1.call-start = ((), (), s32[]{:S(2)}) async-start(), calls=%async_computation.1 | async-start | bytes 25165824 | tf_op jit(solution)/shard_map/psum | solution.py:81
  313.2 25.1 slice-start.15
  321.2 14.5 copy-start.1
  321.8 13.9 copy-start.79
  321.8 16.5 slice-start.16
  352.1 531.3 %all-reduce.22.cloned.1.call-start = ((), (), s32[]{:S(2)}) async-start(), calls=%async_computation.2 | async-start | bytes 25165824 | tf_op jit(solution)/shard_map/psum | solution.py:81
  655.6 494.8 %all-reduce.24.cloned.1.call-start = ((), (), s32[]{:S(2)}) async-start(), calls=%async_computation.3 | async-start | bytes 25165824 | tf_op jit(solution)/shard_map/psum | solution.py:81
  883.4 25.4 slice-start.17
  891.6 14.5 copy-start.5
  892.2 13.9 copy-start.82
  892.2 16.6 slice-start.18
  922.6 227.8 %copy-start.50 = (f32[1536]{0:T(1024)S(1)}, f32[1536]{0:T(1024)}, u32[]{:S(2)}) copy-start(f32[1536]{0:T(1024)} %get-tuple-element.10) | copy-start | bytes 18436
  922.6 530.4 %all-reduce.26.cloned.1.call-start = ((), (), s32[]{:S(2)}) async-start(), calls=%async_computation.4 | async-start | bytes 25165824 | tf_op jit(solution)/shard_map/psum | solution.py:81
  1225.2 494.5 %all-reduce.28.cloned.1.call-start = ((), (), s32[]{:S(2)}) async-start(), calls=%async_computation.5 | async-start | bytes 25165824 | tf_op jit(solution)/shard_map/psum | solution.py:81
  1453.0 25.1 slice-start.19
  1461.0 14.5 copy-start.6
  1461.6 13.9 copy-start.84
  1461.6 16.5 slice-start.20
  1491.9 227.8 %copy-start.53 = (f32[1536]{0:T(1024)S(1)}, f32[1536]{0:T(1024)}, u32[]{:S(2)}) copy-start(f32[1536]{0:T(1024)} %get-tuple-element.7) | copy-start | bytes 18436
  1491.9 531.4 %all-reduce.30.cloned.1.call-start = ((), (), s32[]{:S(2)}) async-start(), calls=%async_computation.6 | async-start | bytes 25165824 | tf_op jit(solution)/shard_map/psum | solution.py:81
  1795.6 4634.7 %all-reduce.32.cloned.1.call-start = ((), (), s32[]{:S(2)}) async-start(), calls=%async_computation.7 | async-start | bytes 56623104 | tf_op jit(solution)/shard_map/psum | solution.py:95
  2023.3 24.6 slice-start.13
  2023.3 24.6 slice-start.21
  2032.1 49.6 copy-start.12
  2032.1 15.8 slice-start.14
  2032.1 15.8 slice-start.22
  2067.0 14.7 copy-start.102
  2067.0 27.8 slice-start.23
  2627.6 49.8 copy-start.42
  3126.9 44.9 slice-start.4
  3134.3 23.0 copy-start.24
  3134.3 37.5 slice-start.5
  3157.3 14.5 copy-start.85
  3157.3 14.5 copy-start.103
  3157.3 28.1 slice-start.25
  3171.8 13.6 slice-start.26
  3171.9 13.6 copy-start.104
  3715.3 49.8 copy-start.43
  3781.6 414.4 %copy-start.51 = (f32[1536]{0:T(1024)S(1)}, f32[1536]{0:T(1024)}, u32[]{:S(2)}) copy-start(f32[1536]{0:T(1024)} %get-tuple-element.10) | copy-start | bytes 18436
  4202.9 44.9 slice-start.2
  4210.3 23.0 copy-start.26
  4210.3 37.6 slice-start.3
  4233.3 14.5 copy-start.83
  4233.3 14.5 copy-start.105
  4233.3 27.9 slice-start.27
  4247.9 13.3 slice-start.28
  4247.9 13.3 copy-start.106
  4789.6 49.8 copy-start.44
  4856.0 412.4 %copy-start.48 = (f32[1536]{0:T(1024)S(1)}, f32[1536]{0:T(1024)}, u32[]{:S(2)}) copy-start(f32[1536]{0:T(1024)} %copy-done.47) | copy-start | bytes 18436
  5282.6 22.4 copy-start.20
  5831.6 49.7 copy-start.52
  5831.7 49.7 copy-start.76
  5881.4 15.7 copy-start.3
  5881.4 15.7 copy-start.49
  5881.4 15.7 copy-start.73
  5881.4 30.6 slice-start.8
  5897.1 15.0 slice-start.9
  5897.1 15.0 copy-start.37
  5941.1 23.8 copy-start.81
  (88 other events, 429.3 us)
Sparse Core Ops, SparseCore 0:
  82.7 230.4 all-reduce.17
  352.2 227.5 all-reduce.19
  655.7 227.6 all-reduce.21
  922.7 227.6 all-reduce.23
  1225.4 227.6 all-reduce.25
  1492.0 227.6 all-reduce.27
  1795.7 227.5 all-reduce.29
  5987.5 77.9 all-reduce.31
where the time goes:
time: 6470 us; the launch traced here: 6460 us
  blocking collectives  3310 us (51%)
  waiting for transfers between devices  1600 us (25%)
  matrix products  1260 us (19%)
  other arithmetic  179 us (3%)
  local copies, waits for them, and re-layouts  93.2 us (1%)
    psum x8, blocking collectives, sum_model(): return lax.psum(values, 'model')  3310 us
    psum x7, waiting for transfers between devices, sum_model(): return lax.psum(values, 'model')  1600 us
    dot_general x4, matrix products, layer_backward(): jnp.einsum('bhqk,bqhe->bkhe', d_scores, q_head, preferred_element_type=jn...  199 us
    dot_general x4, matrix products, layer_backward(): jnp.einsum('bhqk,bkhe->bqhe', d_scores, k_head, preferred_element_type=jn...  198 us
  transfers between devices with their start and end apart: 8, of which 7 were waited for; matrix products, arithmetic and copies ran while one was open for 0% of the time, Pallas kernels for 0%

commit v1 on v0

v1 whole, which is shorter than its diff:
```python
import functools

import jax
import jax.numpy as jnp
from jax import lax
from jax.experimental import pallas as pl
from jax.experimental.pallas import tpu as pltpu
from jax.sharding import PartitionSpec as P

HEAD_DIM = 64
EPS_NORM = 1e-6
F32 = jnp.float32
BF16 = jnp.bfloat16
LOG2E = 1.4426950408889634
SCALE = HEAD_DIM ** -0.5

SWAP_D = [(0, 1), (1, 0)]
SWAP_X = [(0, 1), (1, 0), (2, 3), (3, 2)]
SWAP_Y = [(0, 2), (2, 0), (1, 3), (3, 1)]


def pp_d(v):
    return lax.ppermute(v, 'data', SWAP_D)


def pp_x(v):
    return lax.ppermute(v, 'model', SWAP_X)


def pp_y(v):
    return lax.ppermute(v, 'model', SWAP_Y)


def rms_norm(values):
    return values * lax.rsqrt(jnp.mean(values * values, axis=-1, keepdims=True) + EPS_NORM)


def dot(a, b, dims):
    return lax.dot_general(a, b, (dims, ((), ())), preferred_element_type=F32)


def nn(a, b):
    return dot(a, b, ((1,), (0,)))


def nt(a, b):
    return dot(a, b, ((1,), (1,)))


def tn(a, b):
    return dot(a, b, ((0,), (0,)))


def pair_masks(rows):
    lane = lax.broadcasted_iota(jnp.int32, (rows, 128), 1)
    return lane < HEAD_DIM


def attn_fwd_body(q_ref, ko_ref, ks_ref, vo_ref, vs_ref, ctx_ref, lse_ref):
    k = jnp.concatenate([ko_ref[...], ks_ref[...]], axis=0)
    v = jnp.concatenate([vo_ref[...], vs_ref[...]], axis=0)
    tq = q_ref.shape[0]
    chunk = 256
    low = pair_masks(chunk)
    scores = []
    for i in range(tq // chunk):
        q = q_ref[i * chunk:(i + 1) * chunk, :]
        zero = jnp.zeros_like(q)
        both = jnp.concatenate([jnp.where(low, q, zero), jnp.where(low, zero, q)], axis=0)
        scores.append(nt(k, both))
    for i, s in enumerate(scores):
        rows = slice(i * chunk, (i + 1) * chunk)
        m = jnp.max(s, axis=0, keepdims=True)
        p = jnp.exp2((s - m) * (SCALE * LOG2E))
        l = jnp.sum(p, axis=0, keepdims=True)
        pb = (p * (1.0 / l)).astype(BF16)
        lse = m * (SCALE * LOG2E) + jnp.log2(l)
        lse_ref[0, 0:1, rows] = lse[:, :chunk]
        lse_ref[0, 1:2, rows] = lse[:, chunk:]
        ctx_t = tn(v, pb)
        ctx_t = jnp.concatenate([ctx_t[:HEAD_DIM, :chunk], ctx_t[HEAD_DIM:, chunk:]], axis=0)
        ctx_ref[rows, :] = ctx_t.T.astype(BF16)


def attn_fwd(q, kv, kv_s):
    tq, width = q.shape
    tk = kv.shape[0]
    pairs = width // 128
    def col(off):
        return lambda j: (0, j + off)
    flops = 2 * 2 * tq * (2 * tk) * 256 * (width // HEAD_DIM)
    return pl.pallas_call(
        attn_fwd_body,
        grid=(pairs,),
        in_specs=[pl.BlockSpec((tq, 128), col(0)),
                  pl.BlockSpec((tk, 128), col(0)), pl.BlockSpec((tk, 128), col(0)),
                  pl.BlockSpec((tk, 128), col(pairs)), pl.BlockSpec((tk, 128), col(pairs))],
        out_specs=[pl.BlockSpec((tq, 128), col(0)),
                   pl.BlockSpec((1, 2, tq), lambda j: (j, 0, 0))],
        out_shape=[jax.ShapeDtypeStruct((tq, width), BF16),
                   jax.ShapeDtypeStruct((pairs, 2, tq), F32)],
        compiler_params=pltpu.CompilerParams(dimension_semantics=('arbitrary',),
                                             vmem_limit_bytes=48 * 1024 * 1024),
        cost_estimate=pl.CostEstimate(flops=flops, bytes_accessed=2 * (tq * width * 2 + 4 * tk * width),
                                      transcendentals=tq * 2 * tk * (width // HEAD_DIM)),
        name='attn_fwd',
    )(q, kv, kv_s, kv, kv_s)


def attn_bwd_body(q_ref, ko_ref, ks_ref, vo_ref, vs_ref, do_ref, lse_ref,
                  dq_ref, dko_ref, dks_ref, dvo_ref, dvs_ref):
    tk = ko_ref.shape[0]
    k = jnp.concatenate([ko_ref[...], ks_ref[...]], axis=0)
    v = jnp.concatenate([vo_ref[...], vs_ref[...]], axis=0)
    tq = q_ref.shape[0]
    chunk = 256
    low = pair_masks(chunk)
    for ref in (dko_ref, dks_ref, dvo_ref, dvs_ref):
        ref[...] = jnp.zeros_like(ref)

    def step(i, carry):
        rows = pl.ds(pl.multiple_of(i * chunk, chunk), chunk)
        q = q_ref[rows, :]
        do = do_ref[rows, :]
        lse = lse_ref[0, :, rows]
        dqs = []
        for h in range(2):
            sel = low if h == 0 else ~low
            qm = jnp.where(sel, q, jnp.zeros_like(q))
            dom = jnp.where(sel, do, jnp.zeros_like(do))
            s = nt(k, qm)
            p = jnp.exp2(s * (SCALE * LOG2E) - lse[h:h + 1, :])
            dp = nt(v, dom).astype(BF16).astype(F32)
            delta = jnp.sum(p * dp, axis=0, keepdims=True)
            ds = (p * (dp - delta)).astype(BF16)
            dv = nn(p.astype(BF16), dom)
            dk = nn(ds, qm) * SCALE
            dvo_ref[...] += dv[:tk]
            dvs_ref[...] += dv[tk:]
            dko_ref[...] += dk[:tk]
            dks_ref[...] += dk[tk:]
            dqs.append(tn(k, ds)[h * HEAD_DIM:(h + 1) * HEAD_DIM, :] * SCALE)
        dq_ref[rows, :] = jnp.concatenate(dqs, axis=0).T.astype(BF16)
        return carry

    lax.fori_loop(0, tq // chunk, step, 0)


def attn_bwd(q, kv, kv_s, d_ctx, lse):
    tq, width = q.shape
    tk = kv.shape[0]
    pairs = width // 128
    def col(off):
        return lambda j: (0, j + off)
    flops = 5 * 2 * tq * (2 * tk) * 256 * (width // HEAD_DIM)
    kblk = pl.BlockSpec((tk, 128), col(0))
    return pl.pallas_call(
        attn_bwd_body,
        grid=(pairs,),
        in_specs=[pl.BlockSpec((tq, 128), col(0)),
                  kblk, kblk,
                  pl.BlockSpec((tk, 128), col(pairs)), pl.BlockSpec((tk, 128), col(pairs)),
                  pl.BlockSpec((tq, 128), col(0)),
                  pl.BlockSpec((1, 2, tq), lambda j: (j, 0, 0))],
        out_specs=[pl.BlockSpec((tq, 128), col(0)), kblk, kblk, kblk, kblk],
        out_shape=[jax.ShapeDtypeStruct((tq, width), BF16)]
        + [jax.ShapeDtypeStruct((tk, width), F32)] * 4,
        compiler_params=pltpu.CompilerParams(dimension_semantics=('arbitrary',),
                                             vmem_limit_bytes=48 * 1024 * 1024),
        cost_estimate=pl.CostEstimate(flops=flops, bytes_accessed=2 * (2 * tq * width * 2 + 4 * tk * width) + 16 * tk * width,
                                      transcendentals=tq * 2 * tk * (width // HEAD_DIM)),
        name='attn_bwd',
    )(q, kv, kv_s, kv, kv_s, d_ctx, lse)


def gather_pieces(part_a, part_b):
    xa, xb = pp_x(part_a), pp_x(part_b)
    ya, yb = pp_y(part_a), pp_y(part_b)
    da, db = pp_y(xa), pp_x(yb)
    own = [(part_a, part_b), (xa, xb), (ya, yb), (da, db)]
    sib = [None] + [(pp_d(a), pp_d(b)) for a, b in own[1:]]
    return own, sib


def reduce_pieces(piece):
    total = {}
    for r in (3, 1, 2, 0):
        for part in (0, 1):
            total[r, part] = piece(r, 0, part) + pp_d(piece(r, 1, part))
    a0 = total[0, 0] + pp_x(total[1, 0])
    a2 = total[2, 0] + pp_x(total[3, 0])
    b0 = total[0, 1] + pp_y(total[2, 1])
    b1 = total[1, 1] + pp_y(total[3, 1])
    own = (a0 + pp_y(a2), b0 + pp_x(b1))
    return own, (pp_d(own[0]), pp_d(own[1]))


def solution(mesh):
    spec_col = P(None, 'model')
    spec_row = P('model', None)
    spec_act = P('data', None, None)
    spec_rep = P(None, None)

    def device_step(x_in, cot_out, step_emb, w_q, w_k, w_v, w_o, w_1, w_2):
        layer_count, dim = step_emb.shape
        core = lax.axis_index('data')
        chip = lax.axis_index('model')
        chip_x = lax.rem(chip, 2)
        chip_y = lax.div(chip, 2)
        half_d = dim // 2
        seq = x_in.shape[1]
        half_t = seq // 2

        def ordered(own, sib, axis):
            size = own.shape[axis]
            shape = own.shape[:axis] + (2 * size,) + own.shape[axis + 1:]
            out = lax.dynamic_update_slice_in_dim(jnp.zeros(shape, own.dtype), own, core * size, axis)
            return lax.dynamic_update_slice_in_dim(out, sib, (1 - core) * size, axis)

        def take(v, which, axis, parts=2):
            size = v.shape[axis] // parts
            return lax.dynamic_slice_in_dim(v, which * size, size, axis)

        def my_tokens(v):
            mine = lax.dynamic_index_in_dim(v, chip_x, 0, keepdims=False)
            recv = pp_d(take(mine, 1 - core, 0))
            return jnp.where(core == chip_y, take(mine, core, 0), recv)

        x_cur = my_tokens(x_in)
        d_cur = my_tokens(cot_out)

        w_qkv = jnp.concatenate([w_q, w_k, w_v], axis=1)
        hid = w_q.shape[1]
        own_qkv = take(w_qkv, core, 0)
        quart = half_d // 2
        qkv_own, qkv_sib = gather_pieces(own_qkv[:quart], own_qkv[quart:])
        wqkv = [w_qkv] + [ordered(jnp.concatenate(qkv_own[r], 0), jnp.concatenate(qkv_sib[r], 0), 0) for r in (1, 2, 3)]
        wq = jnp.concatenate([w[:, :hid] for w in wqkv], axis=1)
        wkv = jnp.concatenate([w[:, hid:2 * hid] for w in wqkv] + [w[:, 2 * hid:] for w in wqkv], axis=1)
        own_o = take(w_o, core, 1)
        o_own, o_sib = gather_pieces(own_o[:, :quart], own_o[:, quart:])
        wo = jnp.concatenate([w_o] + [ordered(jnp.concatenate(o_own[r], 1), jnp.concatenate(o_sib[r], 1), 1) for r in (1, 2, 3)], axis=0)

        own_1, sib_1 = take(w_1, core, 1), take(w_1, 1 - core, 1)
        p1_own, p1_sib = gather_pieces(own_1[:half_d], own_1[half_d:])
        w1_list = [own_1, sib_1]
        for r in (1, 2, 3):
            w1_list += [jnp.concatenate(p1_own[r], 0), jnp.concatenate(p1_sib[r], 0)]
        w1 = jnp.concatenate(w1_list, axis=1)
        own_2, sib_2 = take(w_2, core, 0), take(w_2, 1 - core, 0)
        p2_own, p2_sib = gather_pieces(own_2[:, :half_d], own_2[:, half_d:])
        w2_list = [own_2, sib_2]
        for r in (1, 2, 3):
            w2_list += [jnp.concatenate(p2_own[r], 1), jnp.concatenate(p2_sib[r], 1)]
        w2 = jnp.concatenate(w2_list, axis=0)

        saved = []
        for layer in range(layer_count):
            s = x_cur.astype(F32) + step_emb[layer].astype(F32)
            u = rms_norm(s).astype(BF16)
            kv = nn(u, wkv).astype(BF16)
            kv_s = pp_d(kv)
            q = nn(u, wq).astype(BF16)
            ctx, lse = attn_fwd(q, kv, kv_s)
            h = (s + nn(ctx, wo)).astype(BF16)
            m = rms_norm(h.astype(F32)).astype(BF16)
            z = nn(m, w1).astype(BF16)
            g = jax.nn.gelu(z.astype(F32)).astype(BF16)
            x_next = (h.astype(F32) + nn(g, w2)).astype(BF16)
            saved.append((x_cur, u, q, kv, kv_s, ctx, lse, h, m, z, g))
            x_cur = x_next

        hist = []
        for layer in reversed(range(layer_count)):
            x_l, u, q, kv, kv_s, ctx, lse, h, m, z, g = saved[layer]
            d_next = d_cur
            d_act = nt(d_next, w2).astype(BF16)
            gelu_pull = jax.vjp(jax.nn.gelu, z.astype(F32))[1]
            d_up = gelu_pull(d_act.astype(F32))[0].astype(BF16)
            d_norm2 = nt(d_up, w1).astype(BF16)
            norm_pull = jax.vjp(rms_norm, h.astype(F32))[1]
            d_mid = (d_next.astype(F32) + norm_pull(d_norm2.astype(F32))[0]).astype(BF16)
            d_ctx = nt(d_mid, wo).astype(BF16)
            dq, dko, dks, dvo, dvs = attn_bwd(q, kv, kv_s, d_ctx, lse)
            dk = (dko + pp_d(dks)).astype(BF16)
            dv = (dvo + pp_d(dvs)).astype(BF16)
            dkv = jnp.concatenate([dk, dv], axis=1)
            d_norm1 = (nt(dq, wq) + nt(dkv, wkv)).astype(BF16)
            s = x_l.astype(F32) + step_emb[layer].astype(F32)
            norm_pull_x = jax.vjp(rms_norm, s)[1]
            d_cur = (d_mid.astype(F32) + norm_pull_x(d_norm1.astype(F32))[0]).astype(BF16)
            hist.append((u, dq, dkv, ctx, d_mid, m, d_up, g, d_next))

        u_h, dq_h, dkv_h, ctx_h, mid_h, m_h, up_h, g_h, next_h = [jnp.concatenate(v, axis=0) for v in zip(*hist)]
        ff = w_1.shape[1] // 2

        def piece_2(r, half, part):
            col = (2 * r + half) * ff
            return tn(g_h[:, col:col + ff], next_h[:, part * half_d:(part + 1) * half_d])

        def piece_1(r, half, part):
            col = (2 * r + half) * ff
            return tn(m_h[:, part * half_d:(part + 1) * half_d], up_h[:, col:col + ff])

        mid_half = tuple(lax.optimization_barrier(take(mid_h, w, 1)) for w in (core, 1 - core))
        u_half = tuple(lax.optimization_barrier(take(u_h, w, 1)) for w in (core, 1 - core))

        def piece_o(r, half, part):
            return tn(ctx_h[:, r * hid:(r + 1) * hid], mid_half[half][:, part * quart:(part + 1) * quart])

        dqkv_r = [lax.optimization_barrier(jnp.concatenate([dq_h[:, r * hid:(r + 1) * hid], dkv_h[:, r * hid:(r + 1) * hid],
                                   dkv_h[:, (4 + r) * hid:(5 + r) * hid]], axis=1)) for r in range(4)]

        def piece_qkv(r, half, part):
            return tn(u_half[half][:, part * quart:(part + 1) * quart], dqkv_r[r])

        own, sib = reduce_pieces(piece_2)
        grad_2 = ordered(jnp.concatenate(own, 1), jnp.concatenate(sib, 1), 0)
        own, sib = reduce_pieces(piece_1)
        grad_1 = ordered(jnp.concatenate(own, 0), jnp.concatenate(sib, 0), 1)
        own, sib = reduce_pieces(piece_o)
        grad_o = ordered(jnp.concatenate(own, 1), jnp.concatenate(sib, 1), 1)
        own, sib = reduce_pieces(piece_qkv)
        grad_qkv = ordered(jnp.concatenate(own, 0), jnp.concatenate(sib, 0), 0)

        whole = ordered(d_cur, pp_d(d_cur), 0)
        to_row = [(2 * c + d, 2 * (c ^ 2) + d) for c in range(4) for d in range(2) if c // 2 == d]
        from_y = lax.ppermute(whole, ('model', 'data'), to_row)
        row_seq = jnp.where(chip_y == core, whole, from_y)
        other = pp_x(row_seq)
        d_x = jnp.where(chip_x == 0, jnp.stack([row_seq, other]), jnp.stack([other, row_seq]))
        return (grad_qkv[:, :hid], grad_qkv[:, hid:2 * hid], grad_qkv[:, 2 * hid:], grad_o, grad_1, grad_2, d_x)

    return jax.shard_map(device_step, mesh=mesh,
                         in_specs=(spec_act, spec_act, spec_rep, spec_col, spec_col, spec_col, spec_row, spec_col, spec_row),
                         out_specs=(spec_col, spec_col, spec_col, spec_row, spec_col, spec_row, spec_act),
                         check_vma=False)
```

time: 6470 us -> 2090 us (0.32)
  blocking collectives: 3310 us -> 0 us
  waiting for transfers between devices: 1600 us -> 651 us
  matrix products: 1260 us -> 728 us
  Pallas kernels: 0 us -> 292 us
  starting transfers between devices: 0.33 us -> 76.6 us
    psum x8 -> x0, blocking collectives: 3310 us -> none  [sum_model(): return lax.psum(values, 'model')]
    psum x8 -> x0, waiting for transfers between devices: 1600 us -> none  [the longest x7 1600 us: sum_model(): return lax.psum(values, 'model')]
    ppermute x0 -> x129, waiting for transfers between devices: none -> 651 us  [the longest x25 377 us: pp_x(): return lax.ppermute(v, 'model', SWAP_X)]
    dot_general x67 -> x103, matrix products: 1170 us -> 728 us  [dot(): return lax.dot_general(a, b, (dims, ((), ())), preferred_element_type=F32)]
    pallas_call x0 -> x8, Pallas kernels: none -> 292 us  [the longest x4 197 us: attn_bwd(): pl.pallas_call(attn_bwd_body, grid=(pairs,), in_specs=[pl.BlockSpec((tq,...]
    sub x4 -> x0, matrix products: 92.9 us -> none  [attn_probs(): return jax.nn.softmax(scores * HEAD_DIM ** (-0.5), axis=-1)]
    concatenate x0 -> x18, other arithmetic: none -> 88.9 us  [the longest x7 66.1 us: device_step(): jnp.concatenate(v, axis=0)]
    ppermute x0 -> x129, starting transfers between devices: none -> 76.6 us  [the longest x24 30.6 us: pp_y(): return lax.ppermute(v, 'model', SWAP_Y)]
  transfers between devices with their start and end apart: 8 -> 129, of which waited for: 7 -> 40; matrix products, arithmetic and copies ran while one was open for 0% -> 21% of each run, Pallas kernels for 0% -> 2%
where the time goes in v1:
time: 2090 us; the launch traced here: 2080 us
  matrix products  728 us (35%)
  waiting for transfers between devices  651 us (31%)
  Pallas kernels  292 us (14%)
  other arithmetic  213 us (10%)
  local copies, waits for them, and re-layouts  113 us (5%)
  starting transfers between devices  76.6 us (4%)
    dot_general x103, matrix products, dot(): return lax.dot_general(a, b, (dims, ((), ())), preferred_element_type=F32)  728 us
    ppermute x25, waiting for transfers between devices, pp_x(): return lax.ppermute(v, 'model', SWAP_X)  377 us
    ppermute x24, waiting for transfers between devices, pp_y(): return lax.ppermute(v, 'model', SWAP_Y)  244 us
    pallas_call x4, Pallas kernels, attn_bwd(): pl.pallas_call(attn_bwd_body, grid=(pairs,), in_specs=[pl.BlockSpec((tq,...  197 us
    pallas_call x4, Pallas kernels, attn_fwd(): pl.pallas_call(attn_fwd_body, grid=(pairs,), in_specs=[pl.BlockSpec((tq,...  95.2 us
    concatenate x7, other arithmetic, device_step(): jnp.concatenate(v, axis=0)  66.1 us
    unnamed x487, local copies, waits for them, and re-layouts  48.3 us
  transfers between devices with their start and end apart: 129, of which 40 were waited for; matrix products, arithmetic and copies ran while one was open for 21% of the time, Pallas kernels for 2%

profile of v1, /device:TPU:0, one launch (start us, length us, event | category | flops | bytes accessed | tf_op | source)
XLA Modules:
  0.0 2078.7 jit_solution(478047721846475518)
XLA Ops:
  42.0 7.9 collective-permute-done.1
  51.1 17.3 collective-permute-done.2
  80.7 16.5 collective-permute-done.26
  97.2 25.3 %collective-permute-done.27 = bf16[768,768]{1,0:T(8,128)(2,1)S(1)} collective-permute-done((bf16[768,768]{1,0:T(8,128)(2,1)S(1)}, bf16[768,768]{1,0:T(8,128)(2,1)S(1)}, u32[]{:S(2)}, u32[]{:S(2)}) %collective-permute-start.27) | collective-permute-done | bytes 1179680 | tf_op jit(solution)/shard_map/ppermute | solution.py:27
  124.1 23.7 %collective-permute-done.38 = bf16[768,768]{1,0:T(8,128)(2,1)S(1)} collective-permute-done((bf16[768,768]{1,0:T(8,128)(2,1)S(1)}, bf16[768,768]{1,0:T(8,128)(2,1)S(1)}, u32[]{:S(2)}, u32[]{:S(2)}) %collective-permute-start.38) | collective-permute-done | bytes 1179680 | tf_op jit(solution)/shard_map/ppermute | solution.py:27
  147.8 24.1 %collective-permute-done.39 = bf16[768,768]{1,0:T(8,128)(2,1)S(1)} collective-permute-done((bf16[768,768]{1,0:T(8,128)(2,1)S(1)}, bf16[768,768]{1,0:T(8,128)(2,1)S(1)}, u32[]{:S(2)}, u32[]{:S(2)}) %collective-permute-start.39) | collective-permute-done | bytes 1179680 | tf_op jit(solution)/shard_map/ppermute | solution.py:27
  182.5 13.1 collective-permute-done.10
  205.2 21.1 %collective-permute-done.31 = bf16[768,768]{1,0:T(8,128)(2,1)S(1)} collective-permute-done((bf16[768,768]{1,0:T(8,128)(2,1)S(1)}, bf16[768,768]{1,0:T(8,128)(2,1)S(1)}, u32[]{:S(2)}, u32[]{:S(2)}) %collective-permute-start.31) | collective-permute-done | bytes 1179680 | tf_op jit(solution)/shard_map/ppermute | solution.py:31
  227.8 23.8 %collective-permute-done.30 = bf16[768,768]{1,0:T(8,128)(2,1)S(1)} collective-permute-done((bf16[768,768]{1,0:T(8,128)(2,1)S(1)}, bf16[768,768]{1,0:T(8,128)(2,1)S(1)}, u32[]{:S(2)}, u32[]{:S(2)}) %collective-permute-start.30) | collective-permute-done | bytes 1179680 | tf_op jit(solution)/shard_map/ppermute | solution.py:31
  261.9 14.9 collective-permute-done.43
  277.1 25.0 %collective-permute-done.42 = bf16[768,768]{1,0:T(8,128)(2,1)S(1)} collective-permute-done((bf16[768,768]{1,0:T(8,128)(2,1)S(1)}, bf16[768,768]{1,0:T(8,128)(2,1)S(1)}, u32[]{:S(2)}, u32[]{:S(2)}) %collective-permute-start.42) | collective-permute-done | bytes 1179680 | tf_op jit(solution)/shard_map/ppermute | solution.py:31
  302.6 9.4 convolution_convert_fusion.11.ko_ref.vo_ref
  313.6 13.8 collective-permute-done.34
  335.3 16.6 collective-permute-done.46
  365.9 23.8 %attn_fwd.4 = (bf16[512,1536]{1,0:T(8,128)(2,1)S(1)}, f32[12,2,512]{2,1,0:T(2,128)S(1)}) custom-call(bf16[512,1536]{1,0:T(8,128)(2,1)S(1)} %convolution_convert_fusion.19.q_ref, bf16[512,3072]{1,0:T(8,128)(2,1)} %copy-done.193, bf16[512,3072]{1,0:T(8,128)(2,1)} %collective-permute-done.13.ks_ref.vs_ref, bf16[512,3072]{1,0:T(8,128)(2,1)} %copy-done.193, ...), custom_call_target="tpu_custom_call" | custom-call | flops 12884901888 | bytes 9437184 | tf_op jit(solution)/shard_map/attn_fwd/pallas_call | solution.py:92
  393.4 23.0 %fusion.23 = (bf16[512,6144]{1,0:T(8,128)(2,1)}, bf16[512,6144]{1,0:T(8,128)(2,1)}) fusion(bf16[512,1536]{1,0:T(8,128)(2,1)S(1)} %fusion.68, bf16[1536,6144]{1,0:T(8,128)(2,1)} %maximum_dynamic-update-slice_fusion.4), kind=kOutput, calls=%fused_computation.49 | convolution fusion | flops 9698279424 | bytes 33030144 | tf_op jit(solution)/shard_map/dot_general | solution.py:39
  416.4 21.1 %multiply_reduce_fusion.2 = (f32[512]{0:T(512)S(1)}, bf16[512,1536]{1,0:T(8,128)(2,1)S(1)}) fusion(f32[1536]{0:T(1024)S(1)} %get-tuple-element.64, bf16[6144,1536]{1,0:T(8,128)(2,1)} %maximum_dynamic-update-slice_fusion.10, bf16[512,6144]{1,0:T(8,128)(2,1)} %get-tuple-element.133, bf16[512,1536]{1,0:T(8,128)(2,1)S(1)} %get-tuple-element.105), kind=kOutput, calls=%fused_computation.213 | convolution fusion | flops 9700638720 | bytes 28319744 | tf_op jit(solution)/shard_map/dot_general | solution.py:39
  438.1 9.9 convolution_convert_fusion.10.ko_ref.vo_ref
  453.8 23.7 %attn_fwd.5 = (bf16[512,1536]{1,0:T(8,128)(2,1)S(1)}, f32[12,2,512]{2,1,0:T(2,128)S(1)}) custom-call(bf16[512,1536]{1,0:T(8,128)(2,1)S(1)} %convolution_convert_fusion.18.q_ref, bf16[512,3072]{1,0:T(8,128)(2,1)} %copy-done.194, bf16[512,3072]{1,0:T(8,128)(2,1)} %collective-permute-done.50.ks_ref.vs_ref, bf16[512,3072]{1,0:T(8,128)(2,1)} %copy-done.194, ...), custom_call_target="tpu_custom_call" | custom-call | flops 12884901888 | bytes 9437184 | tf_op jit(solution)/shard_map/attn_fwd/pallas_call | solution.py:92
  483.6 22.9 %fusion.29 = (bf16[512,6144]{1,0:T(8,128)(2,1)}, bf16[512,6144]{1,0:T(8,128)(2,1)}) fusion(bf16[512,1536]{1,0:T(8,128)(2,1)S(1)} %fusion.71, bf16[1536,6144]{1,0:T(8,128)(2,1)} %maximum_dynamic-update-slice_fusion.4), kind=kOutput, calls=%fused_computation.55 | convolution fusion | flops 9698279424 | bytes 33030144 | tf_op jit(solution)/shard_map/dot_general | solution.py:39
  506.5 21.5 %multiply_reduce_fusion.1 = (f32[512]{0:T(512)S(1)}, bf16[512,1536]{1,0:T(8,128)(2,1)S(1)}) fusion(f32[1536]{0:T(1024)S(1)} %copy-done.160, bf16[6144,1536]{1,0:T(8,128)(2,1)} %maximum_dynamic-update-slice_fusion.10, bf16[512,6144]{1,0:T(8,128)(2,1)} %get-tuple-element.135, bf16[512,1536]{1,0:T(8,128)(2,1)S(1)} %get-tuple-element.109), kind=kOutput, calls=%fused_computation.210 | convolution fusion | flops 9700638720 | bytes 28319744 | tf_op jit(solution)/shard_map/dot_general | solution.py:39
  528.5 9.6 convolution_convert_fusion.9.ko_ref.vo_ref
  543.8 23.9 %attn_fwd.6 = (bf16[512,1536]{1,0:T(8,128)(2,1)S(1)}, f32[12,2,512]{2,1,0:T(2,128)S(1)}) custom-call(bf16[512,1536]{1,0:T(8,128)(2,1)S(1)} %convolution_convert_fusion.17.q_ref, bf16[512,3072]{1,0:T(8,128)(2,1)} %copy-done.195, bf16[512,3072]{1,0:T(8,128)(2,1)} %collective-permute-done.51.ks_ref.vs_ref, bf16[512,3072]{1,0:T(8,128)(2,1)} %copy-done.195, ...), custom_call_target="tpu_custom_call" | custom-call | flops 12884901888 | bytes 9437184 | tf_op jit(solution)/shard_map/attn_fwd/pallas_call | solution.py:92
  571.4 23.0 %fusion.35 = (bf16[512,6144]{1,0:T(8,128)(2,1)}, bf16[512,6144]{1,0:T(8,128)(2,1)}) fusion(bf16[512,1536]{1,0:T(8,128)(2,1)S(1)} %fusion.74, bf16[1536,6144]{1,0:T(8,128)(2,1)} %maximum_dynamic-update-slice_fusion.4), kind=kOutput, calls=%fused_computation.61 | convolution fusion | flops 9698279424 | bytes 33030144 | tf_op jit(solution)/shard_map/dot_general | solution.py:39
  594.4 21.5 %multiply_reduce_fusion = (f32[512]{0:T(512)S(1)}, bf16[512,1536]{1,0:T(8,128)(2,1)S(1)}) fusion(f32[1536]{0:T(1024)S(1)} %copy-done.162, bf16[6144,1536]{1,0:T(8,128)(2,1)} %maximum_dynamic-update-slice_fusion.10, bf16[512,6144]{1,0:T(8,128)(2,1)} %get-tuple-element.137, bf16[512,1536]{1,0:T(8,128)(2,1)S(1)} %get-tuple-element.113), kind=kOutput, calls=%fused_computation.207 | convolution fusion | flops 9700638720 | bytes 28319744 | tf_op jit(solution)/shard_map/dot_general | solution.py:39
  616.4 9.6 convolution_convert_fusion.8.ko_ref.vo_ref
  639.7 23.9 %attn_fwd.7 = (bf16[512,1536]{1,0:T(8,128)(2,1)S(1)}, f32[12,2,512]{2,1,0:T(2,128)S(1)}) custom-call(bf16[512,1536]{1,0:T(8,128)(2,1)S(1)} %convolution_convert_fusion.16.q_ref, bf16[512,3072]{1,0:T(8,128)(2,1)} %copy-done.196, bf16[512,3072]{1,0:T(8,128)(2,1)} %collective-permute-done.52.ks_ref.vs_ref, bf16[512,3072]{1,0:T(8,128)(2,1)} %copy-done.196, ...), custom_call_target="tpu_custom_call" | custom-call | flops 12884901888 | bytes 9437184 | tf_op jit(solution)/shard_map/attn_fwd/pallas_call | solution.py:92
  667.3 23.1 %fusion.43 = (bf16[512,6144]{1,0:T(8,128)(2,1)}, bf16[512,6144]{1,0:T(8,128)(2,1)}) fusion(bf16[512,1536]{1,0:T(8,128)(2,1)S(1)} %fusion.65, bf16[1536,6144]{1,0:T(8,128)(2,1)} %maximum_dynamic-update-slice_fusion.4), kind=kOutput, calls=%fused_computation.69 | convolution fusion | flops 9698279424 | bytes 33030144 | tf_op jit(solution)/shard_map/dot_general | solution.py:39
  690.4 22.8 %fusion.6 = bf16[512,6144]{1,0:T(8,128)(2,1)} fusion(bf16[512,6144]{1,0:T(8,128)(2,1)} %get-tuple-element.139, bf16[512,1536]{1,0:T(8,128)(2,1)S(1)} %copy-done.22, bf16[6144,1536]{1,0:T(8,128)(2,1)} %maximum_dynamic-update-slice_fusion.10), kind=kOutput, calls=%fused_computation.32 | convolution fusion | flops 9736028160 | bytes 33030144 | tf_op jit(solution)/shard_map/dot_general | solution.py:39
  713.1 16.2 fusion.66
  737.3 49.4 %attn_bwd.4 = (bf16[512,1536]{1,0:T(8,128)(2,1)S(1)}, f32[512,1536]{1,0:T(8,128)}, f32[512,1536]{1,0:T(8,128)}, f32[512,1536]{1,0:T(8,128)}, f32[512,1536]{1,0:T(8,128)}) custom-call(bf16[512,1536]{1,0:T(8,128)(2,1)S(1)} %convolution_convert_fusion.16.q_ref, bf16[512,3072]{1,0:T(8,128)(2,1)} %copy-done.196, ...), custom_call_target="tpu_custom_call" | custom-call | flops 32212254720 | bytes 25165824 | tf_op jit(solution)/shard_map/attn_bwd/pallas_call | solution.py:157
  797.7 8.2 fusion.76
  810.4 23.1 %fusion.9 = bf16[512,6144]{1,0:T(8,128)(2,1)} fusion(bf16[512,6144]{1,0:T(8,128)(2,1)} %get-tuple-element.137, bf16[512,1536]{1,0:T(8,128)(2,1)S(1)} %fusion.51, bf16[6144,1536]{1,0:T(8,128)(2,1)} %maximum_dynamic-update-slice_fusion.10), kind=kOutput, calls=%fused_computation.35 | convolution fusion | flops 9736028160 | bytes 33030144 | tf_op jit(solution)/shard_map/dot_general | solution.py:39
  833.5 16.2 fusion.75
  858.2 49.3 %attn_bwd.5 = (bf16[512,1536]{1,0:T(8,128)(2,1)S(1)}, f32[512,1536]{1,0:T(8,128)}, f32[512,1536]{1,0:T(8,128)}, f32[512,1536]{1,0:T(8,128)}, f32[512,1536]{1,0:T(8,128)}) custom-call(bf16[512,1536]{1,0:T(8,128)(2,1)S(1)} %copy-done.13, bf16[512,3072]{1,0:T(8,128)(2,1)} %copy-done.195, bf16[512,3072]{1,0:T(8,128)(2,1)} %collective-permute-done.51.ks_ref.vs_ref, ...), custom_call_target="tpu_custom_call" | custom-call | flops 32212254720 | bytes 25165824 | tf_op jit(solution)/shard_map/attn_bwd/pallas_call | solution.py:157
  938.2 23.2 %fusion.12 = bf16[512,6144]{1,0:T(8,128)(2,1)} fusion(bf16[512,6144]{1,0:T(8,128)(2,1)} %get-tuple-element.135, bf16[512,1536]{1,0:T(8,128)(2,1)S(1)} %fusion.55, bf16[6144,1536]{1,0:T(8,128)(2,1)} %maximum_dynamic-update-slice_fusion.10), kind=kOutput, calls=%fused_computation.38 | convolution fusion | flops 9736028160 | bytes 33030144 | tf_op jit(solution)/shard_map/dot_general | solution.py:39
  961.4 16.3 fusion.72
  985.7 49.3 %attn_bwd.6 = (bf16[512,1536]{1,0:T(8,128)(2,1)S(1)}, f32[512,1536]{1,0:T(8,128)}, f32[512,1536]{1,0:T(8,128)}, f32[512,1536]{1,0:T(8,128)}, f32[512,1536]{1,0:T(8,128)}) custom-call(bf16[512,1536]{1,0:T(8,128)(2,1)S(1)} %copy-done.11, bf16[512,3072]{1,0:T(8,128)(2,1)} %copy-done.194, bf16[512,3072]{1,0:T(8,128)(2,1)} %collective-permute-done.50.ks_ref.vs_ref, ...), custom_call_target="tpu_custom_call" | custom-call | flops 32212254720 | bytes 25165824 | tf_op jit(solution)/shard_map/attn_bwd/pallas_call | solution.py:157
  1038.4 17.7 pad_maximum_fusion.1
  1064.3 8.2 fusion.84
  1078.3 23.1 %fusion.15 = bf16[512,6144]{1,0:T(8,128)(2,1)} fusion(bf16[512,6144]{1,0:T(8,128)(2,1)} %get-tuple-element.133, bf16[512,1536]{1,0:T(8,128)(2,1)} %fusion.59, bf16[6144,1536]{1,0:T(8,128)(2,1)} %maximum_dynamic-update-slice_fusion.10), kind=kOutput, calls=%fused_computation.41 | convolution fusion | flops 9736028160 | bytes 33030144 | tf_op jit(solution)/shard_map/dot_general | solution.py:39
  1105.5 8.3 fusion.135
  1161.6 15.8 fusion.69
  1177.4 17.9 pad_maximum_fusion
  1282.4 49.3 %attn_bwd.7 = (bf16[512,1536]{1,0:T(8,128)(2,1)S(1)}, f32[512,1536]{1,0:T(8,128)}, f32[512,1536]{1,0:T(8,128)}, f32[512,1536]{1,0:T(8,128)}, f32[512,1536]{1,0:T(8,128)}) custom-call(bf16[512,1536]{1,0:T(8,128)(2,1)S(1)} %copy-done.9, bf16[512,3072]{1,0:T(8,128)(2,1)} %copy-done.193, bf16[512,3072]{1,0:T(8,128)(2,1)} %collective-permute-done.13.ks_ref.vs_ref, ...), custom_call_target="tpu_custom_call" | custom-call | flops 32212254720 | bytes 25165824 | tf_op jit(solution)/shard_map/attn_bwd/pallas_call | solution.py:157
  1349.4 8.5 collective-permute-done.83
  1380.8 8.3 collective-permute-done.87
  1411.5 7.7 fusion.187
  1433.2 7.8 fusion.196
  1470.8 10.0 fusion.88
  1480.9 18.9 maximum_maximum_fusion
  1542.4 34.4 %collective-permute-done.112 = f32[768,768]{0,1:T(8,128)S(1)} collective-permute-done((f32[768,768]{0,1:T(8,128)S(1)}, f32[768,768]{0,1:T(8,128)S(1)}, u32[]{:S(2)}, u32[]{:S(2)}) %collective-permute-start.112) | collective-permute-done | bytes 2359328 | tf_op jit(solution)/shard_map/ppermute | solution.py:27
  1581.9 45.4 %collective-permute-done.115 = f32[768,768]{0,1:T(8,128)S(1)} collective-permute-done((f32[768,768]{0,1:T(8,128)S(1)}, f32[768,768]{0,1:T(8,128)S(1)}, u32[]{:S(2)}, u32[]{:S(2)}) %collective-permute-start.115) | collective-permute-done | bytes 2359328 | tf_op jit(solution)/shard_map/ppermute | solution.py:27
  1644.9 33.0 %collective-permute-done.96 = f32[768,768]{1,0:T(8,128)S(1)} collective-permute-done((f32[768,768]{1,0:T(8,128)}, f32[768,768]{1,0:T(8,128)S(1)}, u32[]{:S(2)}, u32[]{:S(2)}) %collective-permute-start.96) | collective-permute-done | bytes 2359328 | tf_op jit(solution)/shard_map/ppermute | solution.py:27
  1677.9 49.6 %collective-permute-done.99 = f32[768,768]{1,0:T(8,128)} collective-permute-done((f32[768,768]{1,0:T(8,128)}, f32[768,768]{1,0:T(8,128)}, u32[]{:S(2)}, u32[]{:S(2)}) %collective-permute-start.99) | collective-permute-done | bytes 2359328 | tf_op jit(solution)/shard_map/ppermute | solution.py:27
  1760.7 23.9 %collective-permute-done.67 = f32[384,1152]{1,0:T(8,128)} collective-permute-done((f32[384,1152]{1,0:T(8,128)S(1)}, f32[384,1152]{1,0:T(8,128)}, u32[]{:S(2)}, u32[]{:S(2)}) %collective-permute-start.67) | collective-permute-done | bytes 1769504 | tf_op jit(solution)/shard_map/ppermute | solution.py:27
  1791.5 41.9 %collective-permute-done.74 = f32[384,1152]{1,0:T(8,128)} collective-permute-done((f32[384,1152]{1,0:T(8,128)}, f32[384,1152]{1,0:T(8,128)}, u32[]{:S(2)}, u32[]{:S(2)}) %collective-permute-start.74) | collective-permute-done | bytes 1769504 | tf_op jit(solution)/shard_map/ppermute | solution.py:31
  1847.4 36.5 %collective-permute-done.100 = f32[768,768]{1,0:T(8,128)} collective-permute-done((f32[768,768]{1,0:T(8,128)}, f32[768,768]{1,0:T(8,128)}, u32[]{:S(2)}, u32[]{:S(2)}) %collective-permute-start.100) | collective-permute-done | bytes 2359328 | tf_op jit(solution)/shard_map/ppermute | solution.py:31
  1906.0 19.4 collective-permute-done.64
  1925.4 12.3 collective-permute-done.127
  1957.8 15.0 collective-permute-done.71
  1973.5 18.3 collective-permute-done.68
  2049.4 20.5 collective-permute-done.128
  2069.8 8.4 maximum_select_fusion
  (935 shorter events, 707.5 us)
Async XLA Ops:
  28.5 39.9 %collective-permute-start.2 = (bf16[384,1152]{1,0:T(8,128)(2,1)}, bf16[384,1152]{1,0:T(8,128)(2,1)}, u32[]{:S(2)}, u32[]{:S(2)}) collective-permute-start(bf16[384,1152]{1,0:T(8,128)(2,1)} %get-tuple-element.101), channel_id=1, source_target_pairs={{0,2},{2,0},{4,6},{6,4},{1,3},{3,1},{5,7},{7,5}} | collective-permute-start | bytes 2654216 | tf_op jit(solution)/shard_map/ppermute | solution.py:27
  30.9 39.2 %collective-permute-start.6 = (bf16[384,1152]{1,0:T(8,128)(2,1)}, bf16[384,1152]{1,0:T(8,128)(2,1)}, u32[]{:S(2)}, u32[]{:S(2)}) collective-permute-start(bf16[384,1152]{1,0:T(8,128)(2,1)} %get-tuple-element.101), channel_id=1, source_target_pairs={{0,4},{4,0},{2,6},{6,2},{1,5},{5,1},{3,7},{7,3}} | collective-permute-start | bytes 2654216 | tf_op jit(solution)/shard_map/ppermute | solution.py:31
  35.5 36.3 %collective-permute-start.5 = (bf16[384,1152]{1,0:T(8,128)(2,1)}, bf16[384,1152]{1,0:T(8,128)(2,1)}, u32[]{:S(2)}, u32[]{:S(2)}) collective-permute-start(bf16[384,1152]{1,0:T(8,128)(2,1)} %get-tuple-element.100), channel_id=1, source_target_pairs={{0,4},{4,0},{2,6},{6,2},{1,5},{5,1},{3,7},{7,3}} | collective-permute-start | bytes 2654216 | tf_op jit(solution)/shard_map/ppermute | solution.py:31
  70.1 52.4 %collective-permute-start.27 = (bf16[768,768]{1,0:T(8,128)(2,1)S(1)}, bf16[768,768]{1,0:T(8,128)(2,1)S(1)}, u32[]{:S(2)}, u32[]{:S(2)}) collective-permute-start(bf16[768,768]{1,0:T(8,128)(2,1)S(1)} %copy-done.109), channel_id=1, source_target_pairs={{0,2},{2,0},{4,6},{6,4},{1,3},{3,1},{5,7},{7,5}} | collective-permute-start | bytes 3538952 | tf_op jit(solution)/shard_map/ppermute | solution.py:27
  71.7 101.7 %collective-permute-start = (bf16[512,1536]{1,0:T(8,128)(2,1)S(1)}, bf16[512,1536]{1,0:T(8,128)(2,1)S(1)}, u32[]{:S(2)}, u32[]{:S(2)}) collective-permute-start(bf16[512,1536]{1,0:T(8,128)(2,1)S(1)} %dynamic-slice_bitcast_fusion.1), channel_id=1, source_target_pairs={{0,1},{1,0},{2,3},{3,2},{4,5},{5,4},{6,7},{7,6}} | collective-permute-start | bytes 4718600 | tf_op jit(solution)/shard_map/ppermute | solution.py:23
  71.8 76.0 %collective-permute-start.38 = (bf16[768,768]{1,0:T(8,128)(2,1)S(1)}, bf16[768,768]{1,0:T(8,128)(2,1)S(1)}, u32[]{:S(2)}, u32[]{:S(2)}) collective-permute-start(bf16[768,768]{1,0:T(8,128)(2,1)S(1)} %get-tuple-element.90), channel_id=1, source_target_pairs={{0,2},{2,0},{4,6},{6,4},{1,3},{3,1},{5,7},{7,5}} | collective-permute-start | bytes 3538952 | tf_op jit(solution)/shard_map/ppermute | solution.py:27
  73.5 98.3 %collective-permute-start.39 = (bf16[768,768]{1,0:T(8,128)(2,1)S(1)}, bf16[768,768]{1,0:T(8,128)(2,1)S(1)}, u32[]{:S(2)}, u32[]{:S(2)}) collective-permute-start(bf16[768,768]{1,0:T(8,128)(2,1)S(1)} %get-tuple-element.91), channel_id=1, source_target_pairs={{0,2},{2,0},{4,6},{6,4},{1,3},{3,1},{5,7},{7,5}} | collective-permute-start | bytes 3538952 | tf_op jit(solution)/shard_map/ppermute | solution.py:27
  97.2 81.2 %collective-permute-start.3 = (bf16[384,1152]{1,0:T(8,128)(2,1)}, bf16[384,1152]{1,0:T(8,128)(2,1)S(1)}, u32[]{:S(2)}, u32[]{:S(2)}) collective-permute-start(bf16[384,1152]{1,0:T(8,128)(2,1)} %collective-permute-done.1), channel_id=1, source_target_pairs={{0,1},{1,0},{2,3},{3,2},{4,5},{5,4},{6,7},{7,6}} | collective-permute-start | bytes 2654216 | tf_op jit(solution)/shard_map/ppermute | solution.py:23
  122.5 57.5 %collective-permute-start.4 = (bf16[384,1152]{1,0:T(8,128)(2,1)}, bf16[384,1152]{1,0:T(8,128)(2,1)S(1)}, u32[]{:S(2)}, u32[]{:S(2)}) collective-permute-start(bf16[384,1152]{1,0:T(8,128)(2,1)} %collective-permute-done.2), channel_id=1, source_target_pairs={{0,1},{1,0},{2,3},{3,2},{4,5},{5,4},{6,7},{7,6}} | collective-permute-start | bytes 2654216 | tf_op jit(solution)/shard_map/ppermute | solution.py:23
  182.0 44.3 %collective-permute-start.31 = (bf16[768,768]{1,0:T(8,128)(2,1)S(1)}, bf16[768,768]{1,0:T(8,128)(2,1)S(1)}, u32[]{:S(2)}, u32[]{:S(2)}) collective-permute-start(bf16[768,768]{1,0:T(8,128)(2,1)S(1)} %copy-done.109), channel_id=1, source_target_pairs={{0,4},{4,0},{2,6},{6,2},{1,5},{5,1},{3,7},{7,3}} | collective-permute-start | bytes 3538952 | tf_op jit(solution)/shard_map/ppermute | solution.py:31
  195.5 56.0 %collective-permute-start.30 = (bf16[768,768]{1,0:T(8,128)(2,1)S(1)}, bf16[768,768]{1,0:T(8,128)(2,1)S(1)}, u32[]{:S(2)}, u32[]{:S(2)}) collective-permute-start(bf16[768,768]{1,0:T(8,128)(2,1)S(1)} %get-tuple-element.92), channel_id=1, source_target_pairs={{0,4},{4,0},{2,6},{6,2},{1,5},{5,1},{3,7},{7,3}} | collective-permute-start | bytes 3538952 | tf_op jit(solution)/shard_map/ppermute | solution.py:31
  201.0 52.3 %collective-permute-start.11 = (bf16[384,1152]{1,0:T(8,128)(2,1)S(1)}, bf16[384,1152]{1,0:T(8,128)(2,1)S(1)}, u32[]{:S(2)}, u32[]{:S(2)}) collective-permute-start(bf16[384,1152]{1,0:T(8,128)(2,1)S(1)} %collective-permute-done.9), channel_id=1, source_target_pairs={{0,1},{1,0},{2,3},{3,2},{4,5},{5,4},{6,7},{7,6}} | collective-permute-start | bytes 2654216 | tf_op jit(solution)/shard_map/ppermute | solution.py:23
  201.0 52.8 %collective-permute-start.12 = (bf16[384,1152]{1,0:T(8,128)(2,1)S(1)}, bf16[384,1152]{1,0:T(8,128)(2,1)S(1)}, u32[]{:S(2)}, u32[]{:S(2)}) collective-permute-start(bf16[384,1152]{1,0:T(8,128)(2,1)S(1)} %collective-permute-done.10), channel_id=1, source_target_pairs={{0,1},{1,0},{2,3},{3,2},{4,5},{5,4},{6,7},{7,6}} | collective-permute-start | bytes 2654216 | tf_op jit(solution)/shard_map/ppermute | solution.py:23
  202.1 74.8 %collective-permute-start.43 = (bf16[768,768]{1,0:T(8,128)(2,1)S(1)}, bf16[768,768]{1,0:T(8,128)(2,1)S(1)}, u32[]{:S(2)}, u32[]{:S(2)}) collective-permute-start(bf16[768,768]{1,0:T(8,128)(2,1)S(1)} %get-tuple-element.91), channel_id=1, source_target_pairs={{0,4},{4,0},{2,6},{6,2},{1,5},{5,1},{3,7},{7,3}} | collective-permute-start | bytes 3538952 | tf_op jit(solution)/shard_map/ppermute | solution.py:31
  226.3 75.8 %collective-permute-start.42 = (bf16[768,768]{1,0:T(8,128)(2,1)S(1)}, bf16[768,768]{1,0:T(8,128)(2,1)S(1)}, u32[]{:S(2)}, u32[]{:S(2)}) collective-permute-start(bf16[768,768]{1,0:T(8,128)(2,1)S(1)} %get-tuple-element.90), channel_id=1, source_target_pairs={{0,4},{4,0},{2,6},{6,2},{1,5},{5,1},{3,7},{7,3}} | collective-permute-start | bytes 3538952 | tf_op jit(solution)/shard_map/ppermute | solution.py:31
  251.5 50.6 %collective-permute-start.33 = (bf16[768,768]{1,0:T(8,128)(2,1)S(1)}, bf16[768,768]{1,0:T(8,128)(2,1)S(1)}, u32[]{:S(2)}, u32[]{:S(2)}) collective-permute-start(bf16[768,768]{1,0:T(8,128)(2,1)S(1)} %collective-permute-done.31), channel_id=1, source_target_pairs={{0,1},{1,0},{2,3},{3,2},{4,5},{5,4},{6,7},{7,6}} | collective-permute-start | bytes 3538952 | tf_op jit(solution)/shard_map/ppermute | solution.py:23
  253.3 58.8 %collective-permute-start.32 = (bf16[768,768]{1,0:T(8,128)(2,1)S(1)}, bf16[768,768]{1,0:T(8,128)(2,1)S(1)}, u32[]{:S(2)}, u32[]{:S(2)}) collective-permute-start(bf16[768,768]{1,0:T(8,128)(2,1)S(1)} %collective-permute-done.30), channel_id=1, source_target_pairs={{0,1},{1,0},{2,3},{3,2},{4,5},{5,4},{6,7},{7,6}} | collective-permute-start | bytes 3538952 | tf_op jit(solution)/shard_map/ppermute | solution.py:23
  253.8 73.6 %collective-permute-start.34 = (bf16[768,768]{1,0:T(8,128)(2,1)S(1)}, bf16[768,768]{1,0:T(8,128)(2,1)S(1)}, u32[]{:S(2)}, u32[]{:S(2)}) collective-permute-start(bf16[768,768]{1,0:T(8,128)(2,1)S(1)} %collective-permute-done.26), channel_id=1, source_target_pairs={{0,4},{4,0},{2,6},{6,2},{1,5},{5,1},{3,7},{7,3}} | collective-permute-start | bytes 3538952 | tf_op jit(solution)/shard_map/ppermute | solution.py:31
  276.8 50.6 %collective-permute-start.35 = (bf16[768,768]{1,0:T(8,128)(2,1)S(1)}, bf16[768,768]{1,0:T(8,128)(2,1)S(1)}, u32[]{:S(2)}, u32[]{:S(2)}) collective-permute-start(bf16[768,768]{1,0:T(8,128)(2,1)S(1)} %collective-permute-done.31), channel_id=1, source_target_pairs={{0,2},{2,0},{4,6},{6,4},{1,3},{3,1},{5,7},{7,5}} | collective-permute-start | bytes 3538952 | tf_op jit(solution)/shard_map/ppermute | solution.py:27
  312.0 39.9 %collective-permute-start.46 = (bf16[768,768]{1,0:T(8,128)(2,1)S(1)}, bf16[768,768]{1,0:T(8,128)(2,1)S(1)}, u32[]{:S(2)}, u32[]{:S(2)}) collective-permute-start(bf16[768,768]{1,0:T(8,128)(2,1)S(1)} %collective-permute-done.38), channel_id=1, source_target_pairs={{0,4},{4,0},{2,6},{6,2},{1,5},{5,1},{3,7},{7,3}} | collective-permute-start | bytes 3538952 | tf_op jit(solution)/shard_map/ppermute | solution.py:31
  327.9 38.0 %collective-permute-start.13 = (bf16[512,3072]{1,0:T(8,128)(2,1)S(1)}, bf16[512,3072]{1,0:T(8,128)(2,1)}, u32[]{:S(2)}, u32[]{:S(2)}) collective-permute-start(bf16[512,3072]{1,0:T(8,128)(2,1)S(1)} %convolution_convert_fusion.11.ko_ref.vo_ref), channel_id=1, source_target_pairs={{0,1},{1,0},{2,3},{3,2},{4,5},{5,4},{6,7},{7,6}} | collective-permute-start | bytes 9437192 | tf_op jit(solution)/shard_map/ppermute | solution.py:23
  1281.3 130.1 %collective-permute-start.111 = (f32[768,768]{0,1:T(8,128)}, f32[768,768]{0,1:T(8,128)}, u32[]{:S(2)}, u32[]{:S(2)}) collective-permute-start(f32[768,768]{0,1:T(8,128)} %fusion.127), channel_id=1, source_target_pairs={{0,1},{1,0},{2,3},{3,2},{4,5},{5,4},{6,7},{7,6}} | collective-permute-start | bytes 7077896 | tf_op jit(solution)/shard_map/ppermute | solution.py:23
  1281.4 55.2 %collective-permute-start.79 = (f32[384,384]{0,1:T(8,128)S(1)}, f32[384,384]{0,1:T(8,128)}, u32[]{:S(2)}, u32[]{:S(2)}) collective-permute-start(f32[384,384]{0,1:T(8,128)S(1)} %fusion.229), channel_id=1, source_target_pairs={{0,1},{1,0},{2,3},{3,2},{4,5},{5,4},{6,7},{7,6}} | collective-permute-start | bytes 1769480 | tf_op jit(solution)/shard_map/ppermute | solution.py:23
  1281.9 67.5 %collective-permute-start.81 = (f32[384,384]{0,1:T(8,128)S(1)}, f32[384,384]{0,1:T(8,128)S(1)}, u32[]{:S(2)}, u32[]{:S(2)}) collective-permute-start(f32[384,384]{0,1:T(8,128)S(1)} %fusion.224), channel_id=1, source_target_pairs={{0,1},{1,0},{2,3},{3,2},{4,5},{5,4},{6,7},{7,6}} | collective-permute-start | bytes 1769480 | tf_op jit(solution)/shard_map/ppermute | solution.py:23
  1281.9 57.8 %collective-permute-start.82 = (f32[384,384]{0,1:T(8,128)S(1)}, f32[384,384]{0,1:T(8,128)S(1)}, u32[]{:S(2)}, u32[]{:S(2)}) collective-permute-start(f32[384,384]{0,1:T(8,128)S(1)} %fusion.219), channel_id=1, source_target_pairs={{0,1},{1,0},{2,3},{3,2},{4,5},{5,4},{6,7},{7,6}} | collective-permute-start | bytes 1769480 | tf_op jit(solution)/shard_map/ppermute | solution.py:23
  1282.4 62.6 %collective-permute-start.86 = (f32[384,384]{0,1:T(8,128)S(1)}, f32[384,384]{0,1:T(8,128)S(1)}, u32[]{:S(2)}, u32[]{:S(2)}) collective-permute-start(f32[384,384]{0,1:T(8,128)S(1)} %fusion.209), channel_id=1, source_target_pairs={{0,1},{1,0},{2,3},{3,2},{4,5},{5,4},{6,7},{7,6}} | collective-permute-start | bytes 1769480 | tf_op jit(solution)/shard_map/ppermute | solution.py:23
  1377.0 42.3 %collective-permute-start.114 = (f32[768,768]{0,1:T(8,128)}, f32[768,768]{0,1:T(8,128)}, u32[]{:S(2)}, u32[]{:S(2)}) collective-permute-start(f32[768,768]{0,1:T(8,128)} %fusion.111), channel_id=1, source_target_pairs={{0,1},{1,0},{2,3},{3,2},{4,5},{5,4},{6,7},{7,6}} | collective-permute-start | bytes 7077896 | tf_op jit(solution)/shard_map/ppermute | solution.py:23
  1380.3 45.8 %collective-permute-start.118 = (f32[768,768]{0,1:T(8,128)}, f32[768,768]{0,1:T(8,128)}, u32[]{:S(2)}, u32[]{:S(2)}) collective-permute-start(f32[768,768]{0,1:T(8,128)} %fusion.117), channel_id=1, source_target_pairs={{0,1},{1,0},{2,3},{3,2},{4,5},{5,4},{6,7},{7,6}} | collective-permute-start | bytes 7077896 | tf_op jit(solution)/shard_map/ppermute | solution.py:23
  1403.4 59.9 %collective-permute-start.60 = (f32[512,1536]{1,0:T(8,128)}, f32[512,1536]{1,0:T(8,128)}, u32[]{:S(2)}, u32[]{:S(2)}) collective-permute-start(f32[512,1536]{1,0:T(8,128)} %get-tuple-element.60), channel_id=1, source_target_pairs={{0,1},{1,0},{2,3},{3,2},{4,5},{5,4},{6,7},{7,6}} | collective-permute-start | bytes 9437192 | tf_op jit(solution)/shard_map/ppermute | solution.py:23
  1446.3 67.7 %collective-permute-start.110 = (f32[768,768]{0,1:T(8,128)}, f32[768,768]{0,1:T(8,128)}, u32[]{:S(2)}, u32[]{:S(2)}) collective-permute-start(f32[768,768]{0,1:T(8,128)} %fusion.135), channel_id=1, source_target_pairs={{0,1},{1,0},{2,3},{3,2},{4,5},{5,4},{6,7},{7,6}} | collective-permute-start | bytes 7077896 | tf_op jit(solution)/shard_map/ppermute | solution.py:23
  1452.2 64.6 %collective-permute-start.113 = (f32[768,768]{0,1:T(8,128)}, f32[768,768]{0,1:T(8,128)}, u32[]{:S(2)}, u32[]{:S(2)}) collective-permute-start(f32[768,768]{0,1:T(8,128)} %fusion.119), channel_id=1, source_target_pairs={{0,1},{1,0},{2,3},{3,2},{4,5},{5,4},{6,7},{7,6}} | collective-permute-start | bytes 7077896 | tf_op jit(solution)/shard_map/ppermute | solution.py:23
  1457.6 60.5 %collective-permute-start.117 = (f32[768,768]{0,1:T(8,128)}, f32[768,768]{0,1:T(8,128)}, u32[]{:S(2)}, u32[]{:S(2)}) collective-permute-start(f32[768,768]{0,1:T(8,128)} %fusion.133), channel_id=1, source_target_pairs={{0,1},{1,0},{2,3},{3,2},{4,5},{5,4},{6,7},{7,6}} | collective-permute-start | bytes 7077896 | tf_op jit(solution)/shard_map/ppermute | solution.py:23
  1463.3 59.3 %collective-permute-start.120 = (f32[768,768]{0,1:T(8,128)}, f32[768,768]{0,1:T(8,128)}, u32[]{:S(2)}, u32[]{:S(2)}) collective-permute-start(f32[768,768]{0,1:T(8,128)} %fusion.125), channel_id=1, source_target_pairs={{0,1},{1,0},{2,3},{3,2},{4,5},{5,4},{6,7},{7,6}} | collective-permute-start | bytes 7077896 | tf_op jit(solution)/shard_map/ppermute | solution.py:23
  1466.8 61.0 %collective-permute-start.94 = (f32[768,768]{1,0:T(8,128)}, f32[768,768]{1,0:T(8,128)}, u32[]{:S(2)}, u32[]{:S(2)}) collective-permute-start(f32[768,768]{1,0:T(8,128)} %fusion.167), channel_id=1, source_target_pairs={{0,1},{1,0},{2,3},{3,2},{4,5},{5,4},{6,7},{7,6}} | collective-permute-start | bytes 7077896 | tf_op jit(solution)/shard_map/ppermute | solution.py:23
  1522.6 54.1 %collective-permute-start.112 = (f32[768,768]{0,1:T(8,128)S(1)}, f32[768,768]{0,1:T(8,128)S(1)}, u32[]{:S(2)}, u32[]{:S(2)}) collective-permute-start(f32[768,768]{0,1:T(8,128)S(1)} %copy-done.197), channel_id=1, source_target_pairs={{0,2},{2,0},{4,6},{6,4},{1,3},{3,1},{5,7},{7,5}} | collective-permute-start | bytes 7077896 | tf_op jit(solution)/shard_map/ppermute | solution.py:27
  1527.9 99.5 %collective-permute-start.115 = (f32[768,768]{0,1:T(8,128)S(1)}, f32[768,768]{0,1:T(8,128)S(1)}, u32[]{:S(2)}, u32[]{:S(2)}) collective-permute-start(f32[768,768]{0,1:T(8,128)S(1)} %copy-done.198), channel_id=1, source_target_pairs={{0,2},{2,0},{4,6},{6,4},{1,3},{3,1},{5,7},{7,5}} | collective-permute-start | bytes 7077896 | tf_op jit(solution)/shard_map/ppermute | solution.py:27
  1531.7 101.1 %collective-permute-start.119 = (f32[768,768]{0,1:T(8,128)S(1)}, f32[768,768]{0,1:T(8,128)S(1)}, u32[]{:S(2)}, u32[]{:S(2)}) collective-permute-start(f32[768,768]{0,1:T(8,128)S(1)} %copy-done.199), channel_id=1, source_target_pairs={{0,4},{4,0},{2,6},{6,2},{1,5},{5,1},{3,7},{7,3}} | collective-permute-start | bytes 7077896 | tf_op jit(solution)/shard_map/ppermute | solution.py:31
  1536.9 100.7 %collective-permute-start.122 = (f32[768,768]{0,1:T(8,128)}, f32[768,768]{0,1:T(8,128)}, u32[]{:S(2)}, u32[]{:S(2)}) collective-permute-start(f32[768,768]{0,1:T(8,128)} %fusion.196), channel_id=1, source_target_pairs={{0,4},{4,0},{2,6},{6,2},{1,5},{5,1},{3,7},{7,3}} | collective-permute-start | bytes 7077896 | tf_op jit(solution)/shard_map/ppermute | solution.py:31
  1540.7 137.2 %collective-permute-start.96 = (f32[768,768]{1,0:T(8,128)}, f32[768,768]{1,0:T(8,128)S(1)}, u32[]{:S(2)}, u32[]{:S(2)}) collective-permute-start(f32[768,768]{1,0:T(8,128)} %fusion.175), channel_id=1, source_target_pairs={{0,2},{2,0},{4,6},{6,4},{1,3},{3,1},{5,7},{7,5}} | collective-permute-start | bytes 7077896 | tf_op jit(solution)/shard_map/ppermute | solution.py:27
  1576.8 150.7 %collective-permute-start.99 = (f32[768,768]{1,0:T(8,128)}, f32[768,768]{1,0:T(8,128)}, u32[]{:S(2)}, u32[]{:S(2)}) collective-permute-start(f32[768,768]{1,0:T(8,128)} %fusion.181), channel_id=1, source_target_pairs={{0,2},{2,0},{4,6},{6,4},{1,3},{3,1},{5,7},{7,5}} | collective-permute-start | bytes 7077896 | tf_op jit(solution)/shard_map/ppermute | solution.py:27
  1627.3 105.8 %collective-permute-start.106 = (f32[768,768]{1,0:T(8,128)}, f32[768,768]{1,0:T(8,128)}, u32[]{:S(2)}, u32[]{:S(2)}) collective-permute-start(f32[768,768]{1,0:T(8,128)} %fusion.184), channel_id=1, source_target_pairs={{0,4},{4,0},{2,6},{6,2},{1,5},{5,1},{3,7},{7,3}} | collective-permute-start | bytes 7077896 | tf_op jit(solution)/shard_map/ppermute | solution.py:31
  1632.8 104.3 %collective-permute-start.103 = (f32[768,768]{1,0:T(8,128)}, f32[768,768]{1,0:T(8,128)}, u32[]{:S(2)}, u32[]{:S(2)}) collective-permute-start(f32[768,768]{1,0:T(8,128)} %fusion.178), channel_id=1, source_target_pairs={{0,4},{4,0},{2,6},{6,2},{1,5},{5,1},{3,7},{7,3}} | collective-permute-start | bytes 7077896 | tf_op jit(solution)/shard_map/ppermute | solution.py:31
  1637.7 99.4 %collective-permute-start.66 = (f32[384,1152]{1,0:T(8,128)}, f32[384,1152]{1,0:T(8,128)}, u32[]{:S(2)}, u32[]{:S(2)}) collective-permute-start(f32[384,1152]{1,0:T(8,128)} %fusion.257), channel_id=1, source_target_pairs={{0,1},{1,0},{2,3},{3,2},{4,5},{5,4},{6,7},{7,6}} | collective-permute-start | bytes 5308424 | tf_op jit(solution)/shard_map/ppermute | solution.py:23
  1677.9 63.4 %collective-permute-start.63 = (f32[384,1152]{1,0:T(8,128)}, f32[384,1152]{1,0:T(8,128)}, u32[]{:S(2)}, u32[]{:S(2)}) collective-permute-start(f32[384,1152]{1,0:T(8,128)} %fusion.261), channel_id=1, source_target_pairs={{0,1},{1,0},{2,3},{3,2},{4,5},{5,4},{6,7},{7,6}} | collective-permute-start | bytes 5308424 | tf_op jit(solution)/shard_map/ppermute | solution.py:23
  1741.3 92.1 %collective-permute-start.116 = (f32[768,768]{0,1:T(8,128)S(1)}, f32[768,768]{0,1:T(8,128)S(1)}, u32[]{:S(2)}, u32[]{:S(2)}) collective-permute-start(f32[768,768]{0,1:T(8,128)S(1)} %copy-done.104), channel_id=1, source_target_pairs={{0,4},{4,0},{2,6},{6,2},{1,5},{5,1},{3,7},{7,3}} | collective-permute-start | bytes 7077896 | tf_op jit(solution)/shard_map/ppermute | solution.py:31
  1743.1 41.5 %collective-permute-start.67 = (f32[384,1152]{1,0:T(8,128)S(1)}, f32[384,1152]{1,0:T(8,128)}, u32[]{:S(2)}, u32[]{:S(2)}) collective-permute-start(f32[384,1152]{1,0:T(8,128)S(1)} %convolution_add_fusion.12), channel_id=1, source_target_pairs={{0,2},{2,0},{4,6},{6,4},{1,3},{3,1},{5,7},{7,5}} | collective-permute-start | bytes 5308424 | tf_op jit(solution)/shard_map/ppermute | solution.py:27
  1749.5 83.9 %collective-permute-start.74 = (f32[384,1152]{1,0:T(8,128)}, f32[384,1152]{1,0:T(8,128)}, u32[]{:S(2)}, u32[]{:S(2)}) collective-permute-start(f32[384,1152]{1,0:T(8,128)} %convolution_add_fusion.8), channel_id=1, source_target_pairs={{0,4},{4,0},{2,6},{6,2},{1,5},{5,1},{3,7},{7,3}} | collective-permute-start | bytes 5308424 | tf_op jit(solution)/shard_map/ppermute | solution.py:31
  1754.9 92.5 %collective-permute-start.123 = (f32[768,768]{0,1:T(8,128)S(1)}, f32[768,768]{0,1:T(8,128)}, u32[]{:S(2)}, u32[]{:S(2)}) collective-permute-start(f32[768,768]{0,1:T(8,128)S(1)} %add_add_fusion.8), channel_id=1, source_target_pairs={{0,2},{2,0},{4,6},{6,4},{1,3},{3,1},{5,7},{7,5}} | collective-permute-start | bytes 7077896 | tf_op jit(solution)/shard_map/ppermute | solution.py:27
  1755.2 128.7 %collective-permute-start.100 = (f32[768,768]{1,0:T(8,128)}, f32[768,768]{1,0:T(8,128)}, u32[]{:S(2)}, u32[]{:S(2)}) collective-permute-start(f32[768,768]{1,0:T(8,128)} %add_add_fusion.14), channel_id=1, source_target_pairs={{0,4},{4,0},{2,6},{6,2},{1,5},{5,1},{3,7},{7,3}} | collective-permute-start | bytes 7077896 | tf_op jit(solution)/shard_map/ppermute | solution.py:31
  1784.5 110.4 %collective-permute-start.107 = (f32[768,768]{1,0:T(8,128)S(1)}, f32[768,768]{1,0:T(8,128)}, u32[]{:S(2)}, u32[]{:S(2)}) collective-permute-start(f32[768,768]{1,0:T(8,128)S(1)} %add_add_fusion.12), channel_id=1, source_target_pairs={{0,2},{2,0},{4,6},{6,4},{1,3},{3,1},{5,7},{7,5}} | collective-permute-start | bytes 7077896 | tf_op jit(solution)/shard_map/ppermute | solution.py:27
  1833.4 61.1 %collective-permute-start.62 = (f32[384,1152]{1,0:T(8,128)}, f32[384,1152]{1,0:T(8,128)}, u32[]{:S(2)}, u32[]{:S(2)}) collective-permute-start(f32[384,1152]{1,0:T(8,128)} %fusion.263), channel_id=1, source_target_pairs={{0,1},{1,0},{2,3},{3,2},{4,5},{5,4},{6,7},{7,6}} | collective-permute-start | bytes 5308424 | tf_op jit(solution)/shard_map/ppermute | solution.py:23
  1833.4 104.4 %collective-permute-start.127 = (bf16[1024,1536]{1,0:T(8,128)(2,1)S(1)}, bf16[1024,1536]{1,0:T(8,128)(2,1)S(1)}, u32[]{:S(2)}, u32[]{:S(2)}) collective-permute-start(bf16[1024,1536]{1,0:T(8,128)(2,1)S(1)} %constant_dynamic-update-slice_fusion.10), channel_id=1, source_target_pairs={{0,4},{2,6},{5,1},{7,3}} | collective-permute-start | bytes 9437192 | tf_op jit(solution)/shard_map/ppermute | solution.py:328
  1847.4 58.3 %collective-permute-start.69 = (f32[384,1152]{1,0:T(8,128)}, f32[384,1152]{1,0:T(8,128)S(1)}, u32[]{:S(2)}, u32[]{:S(2)}) collective-permute-start(f32[384,1152]{1,0:T(8,128)} %fusion.251), channel_id=1, source_target_pairs={{0,1},{1,0},{2,3},{3,2},{4,5},{5,4},{6,7},{7,6}} | collective-permute-start | bytes 5308424 | tf_op jit(solution)/shard_map/ppermute | solution.py:23
  1883.9 41.5 %collective-permute-start.64 = (f32[384,1152]{1,0:T(8,128)S(1)}, f32[384,1152]{1,0:T(8,128)}, u32[]{:S(2)}, u32[]{:S(2)}) collective-permute-start(f32[384,1152]{1,0:T(8,128)S(1)} %copy-done.107), channel_id=1, source_target_pairs={{0,2},{2,0},{4,6},{6,4},{1,3},{3,1},{5,7},{7,5}} | collective-permute-start | bytes 5308424 | tf_op jit(solution)/shard_map/ppermute | solution.py:27
  1894.4 78.4 %collective-permute-start.71 = (f32[384,1152]{1,0:T(8,128)}, f32[384,1152]{1,0:T(8,128)}, u32[]{:S(2)}, u32[]{:S(2)}) collective-permute-start(f32[384,1152]{1,0:T(8,128)} %convolution_add_fusion.10), channel_id=1, source_target_pairs={{0,4},{4,0},{2,6},{6,2},{1,5},{5,1},{3,7},{7,3}} | collective-permute-start | bytes 5308424 | tf_op jit(solution)/shard_map/ppermute | solution.py:31
  1895.0 96.8 %collective-permute-start.68 = (f32[384,1152]{1,0:T(8,128)}, f32[384,1152]{1,0:T(8,128)}, u32[]{:S(2)}, u32[]{:S(2)}) collective-permute-start(f32[384,1152]{1,0:T(8,128)} %fusion.95), channel_id=1, source_target_pairs={{0,4},{4,0},{2,6},{6,2},{1,5},{5,1},{3,7},{7,3}} | collective-permute-start | bytes 5308424 | tf_op jit(solution)/shard_map/ppermute | solution.py:31
  1905.7 94.1 %collective-permute-start.75 = (f32[384,1152]{1,0:T(8,128)}, f32[384,1152]{1,0:T(8,128)}, u32[]{:S(2)}, u32[]{:S(2)}) collective-permute-start(f32[384,1152]{1,0:T(8,128)} %fusion.92), channel_id=1, source_target_pairs={{0,2},{2,0},{4,6},{6,4},{1,3},{3,1},{5,7},{7,5}} | collective-permute-start | bytes 5308424 | tf_op jit(solution)/shard_map/ppermute | solution.py:27
  1925.4 81.6 %collective-permute-start.124 = (f32[768,768]{0,1:T(8,128)}, f32[768,768]{0,1:T(8,128)}, u32[]{:S(2)}, u32[]{:S(2)}) collective-permute-start(f32[768,768]{0,1:T(8,128)} %add_add_fusion.11), channel_id=1, source_target_pairs={{0,1},{1,0},{2,3},{3,2},{4,5},{5,4},{6,7},{7,6}} | collective-permute-start | bytes 7077896 | tf_op jit(solution)/shard_map/ppermute | solution.py:23
  1937.7 69.3 %collective-permute-start.125 = (f32[768,768]{0,1:T(8,128)}, f32[768,768]{0,1:T(8,128)}, u32[]{:S(2)}, u32[]{:S(2)}) collective-permute-start(f32[768,768]{0,1:T(8,128)} %add_add_fusion.9), channel_id=1, source_target_pairs={{0,1},{1,0},{2,3},{3,2},{4,5},{5,4},{6,7},{7,6}} | collective-permute-start | bytes 7077896 | tf_op jit(solution)/shard_map/ppermute | solution.py:23
  1972.8 63.4 %collective-permute-start.108 = (f32[768,768]{1,0:T(8,128)}, f32[768,768]{1,0:T(8,128)}, u32[]{:S(2)}, u32[]{:S(2)}) collective-permute-start(f32[768,768]{1,0:T(8,128)} %add_add_fusion.15), channel_id=1, source_target_pairs={{0,1},{1,0},{2,3},{3,2},{4,5},{5,4},{6,7},{7,6}} | collective-permute-start | bytes 7077896 | tf_op jit(solution)/shard_map/ppermute | solution.py:23
  1991.7 44.5 %collective-permute-start.109 = (f32[768,768]{1,0:T(8,128)}, f32[768,768]{1,0:T(8,128)}, u32[]{:S(2)}, u32[]{:S(2)}) collective-permute-start(f32[768,768]{1,0:T(8,128)} %add_add_fusion.13), channel_id=1, source_target_pairs={{0,1},{1,0},{2,3},{3,2},{4,5},{5,4},{6,7},{7,6}} | collective-permute-start | bytes 7077896 | tf_op jit(solution)/shard_map/ppermute | solution.py:23
  1999.8 70.0 %collective-permute-start.128 = (bf16[1024,1536]{1,0:T(8,128)(2,1)}, bf16[1024,1536]{1,0:T(8,128)(2,1)}, u32[]{:S(2)}, u32[]{:S(2)}) collective-permute-start(bf16[1024,1536]{1,0:T(8,128)(2,1)} %broadcast_select_fusion), channel_id=1, source_target_pairs={{0,2},{2,0},{4,6},{6,4},{1,3},{3,1},{5,7},{7,5}} | collective-permute-start | bytes 9437192 | tf_op jit(solution)/shard_map/ppermute | solution.py:27
  2007.0 34.1 %collective-permute-start.76 = (f32[384,1152]{1,0:T(8,128)}, f32[384,1152]{1,0:T(8,128)S(1)}, u32[]{:S(2)}, u32[]{:S(2)}) collective-permute-start(f32[384,1152]{1,0:T(8,128)} %fusion.97), channel_id=1, source_target_pairs={{0,1},{1,0},{2,3},{3,2},{4,5},{5,4},{6,7},{7,6}} | collective-permute-start | bytes 5308424 | tf_op jit(solution)/shard_map/ppermute | solution.py:23
  2007.0 34.1 %collective-permute-start.77 = (f32[384,1152]{1,0:T(8,128)}, f32[384,1152]{1,0:T(8,128)S(1)}, u32[]{:S(2)}, u32[]{:S(2)}) collective-permute-start(f32[384,1152]{1,0:T(8,128)} %fusion.94), channel_id=1, source_target_pairs={{0,1},{1,0},{2,3},{3,2},{4,5},{5,4},{6,7},{7,6}} | collective-permute-start | bytes 5308424 | tf_op jit(solution)/shard_map/ppermute | solution.py:23
  (300 other events, 7423.2 us)

commit v2 on v1

v2 whole, which is shorter than its diff:
```python
import jax
import jax.numpy as jnp
from jax import lax
from jax.experimental import pallas as pl
from jax.experimental.pallas import tpu as pltpu
from jax.sharding import PartitionSpec as P


HEAD_DIM = 64
EPS_NORM = 1e-6
F32 = jnp.float32
BF16 = jnp.bfloat16
LOG2E = 1.4426950408889634
SCALE = HEAD_DIM ** -0.5

SWAP_D = [(0, 1), (1, 0)]


def pp_d(v):
    return lax.ppermute(v, 'data', SWAP_D)


def rms_norm(values):
    return values * lax.rsqrt(jnp.mean(values * values, axis=-1, keepdims=True) + EPS_NORM)


def dot(a, b, dims):
    return lax.dot_general(a, b, (dims, ((), ())), preferred_element_type=F32)


def nn(a, b):
    return dot(a, b, ((1,), (0,)))


def nt(a, b):
    return dot(a, b, ((1,), (1,)))


def tn(a, b):
    return dot(a, b, ((0,), (0,)))


def pair_masks(rows):
    lane = lax.broadcasted_iota(jnp.int32, (rows, 128), 1)
    return lane < HEAD_DIM


def attn_fwd_body(q_ref, ko_ref, ks_ref, vo_ref, vs_ref, ctx_ref, lse_ref):
    k = jnp.concatenate([ko_ref[...], ks_ref[...]], axis=0)
    v = jnp.concatenate([vo_ref[...], vs_ref[...]], axis=0)
    tq = q_ref.shape[0]
    chunk = 256
    low = pair_masks(chunk)
    scores = []
    for i in range(tq // chunk):
        q = q_ref[i * chunk:(i + 1) * chunk, :]
        zero = jnp.zeros_like(q)
        both = jnp.concatenate([jnp.where(low, q, zero), jnp.where(low, zero, q)], axis=0)
        scores.append(nt(k, both))
    for i, s in enumerate(scores):
        rows = slice(i * chunk, (i + 1) * chunk)
        m = jnp.max(s, axis=0, keepdims=True)
        p = jnp.exp2((s - m) * (SCALE * LOG2E))
        l = jnp.sum(p, axis=0, keepdims=True)
        pb = (p * (1.0 / l)).astype(BF16)
        lse = m * (SCALE * LOG2E) + jnp.log2(l)
        lse_ref[0, 0:1, rows] = lse[:, :chunk]
        lse_ref[0, 1:2, rows] = lse[:, chunk:]
        ctx_t = tn(v, pb)
        ctx_t = jnp.concatenate([ctx_t[:HEAD_DIM, :chunk], ctx_t[HEAD_DIM:, chunk:]], axis=0)
        ctx_ref[rows, :] = ctx_t.T.astype(BF16)


def attn_fwd(q, kv, kv_s):
    tq, width = q.shape
    tk = kv.shape[0]
    pairs = width // 128

    def col(off):
        return lambda j: (0, j + off)

    flops = 2 * 2 * tq * (2 * tk) * 256 * (width // HEAD_DIM)
    return pl.pallas_call(
        attn_fwd_body,
        grid=(pairs,),
        in_specs=[pl.BlockSpec((tq, 128), col(0)),
                  pl.BlockSpec((tk, 128), col(0)), pl.BlockSpec((tk, 128), col(0)),
                  pl.BlockSpec((tk, 128), col(pairs)), pl.BlockSpec((tk, 128), col(pairs))],
        out_specs=[pl.BlockSpec((tq, 128), col(0)),
                   pl.BlockSpec((1, 2, tq), lambda j: (j, 0, 0))],
        out_shape=[jax.ShapeDtypeStruct((tq, width), BF16),
                   jax.ShapeDtypeStruct((pairs, 2, tq), F32)],
        compiler_params=pltpu.CompilerParams(dimension_semantics=('arbitrary',),
                                             vmem_limit_bytes=48 * 1024 * 1024),
        cost_estimate=pl.CostEstimate(flops=flops, bytes_accessed=2 * (tq * width * 2 + 4 * tk * width),
                                      transcendentals=tq * 2 * tk * (width // HEAD_DIM)),
        name='attn_fwd',
    )(q, kv, kv_s, kv, kv_s)


def attn_bwd_body(q_ref, ko_ref, ks_ref, vo_ref, vs_ref, do_ref, lse_ref,
                  dq_ref, dko_ref, dks_ref, dvo_ref, dvs_ref):
    tk = ko_ref.shape[0]
    k = jnp.concatenate([ko_ref[...], ks_ref[...]], axis=0)
    v = jnp.concatenate([vo_ref[...], vs_ref[...]], axis=0)
    tq = q_ref.shape[0]
    chunk = 256
    low = pair_masks(chunk)
    for ref in (dko_ref, dks_ref, dvo_ref, dvs_ref):
        ref[...] = jnp.zeros_like(ref)

    def step(i, carry):
        rows = pl.ds(pl.multiple_of(i * chunk, chunk), chunk)
        q = q_ref[rows, :]
        do = do_ref[rows, :]
        lse = lse_ref[0, :, rows]
        dqs = []
        for h in range(2):
            sel = low if h == 0 else ~low
            qm = jnp.where(sel, q, jnp.zeros_like(q))
            dom = jnp.where(sel, do, jnp.zeros_like(do))
            s = nt(k, qm)
            p = jnp.exp2(s * (SCALE * LOG2E) - lse[h:h + 1, :])
            dp = nt(v, dom).astype(BF16).astype(F32)
            delta = jnp.sum(p * dp, axis=0, keepdims=True)
            ds = (p * (dp - delta)).astype(BF16)
            dv = nn(p.astype(BF16), dom)
            dk = nn(ds, qm) * SCALE
            dvo_ref[...] += dv[:tk]
            dvs_ref[...] += dv[tk:]
            dko_ref[...] += dk[:tk]
            dks_ref[...] += dk[tk:]
            dqs.append(tn(k, ds)[h * HEAD_DIM:(h + 1) * HEAD_DIM, :] * SCALE)
        dq_ref[rows, :] = jnp.concatenate(dqs, axis=0).T.astype(BF16)
        return carry

    lax.fori_loop(0, tq // chunk, step, 0)


def attn_bwd(q, kv, kv_s, d_ctx, lse):
    tq, width = q.shape
    tk = kv.shape[0]
    pairs = width // 128

    def col(off):
        return lambda j: (0, j + off)

    flops = 5 * 2 * tq * (2 * tk) * 256 * (width // HEAD_DIM)
    kblk = pl.BlockSpec((tk, 128), col(0))
    return pl.pallas_call(
        attn_bwd_body,
        grid=(pairs,),
        in_specs=[pl.BlockSpec((tq, 128), col(0)),
                  kblk, kblk,
                  pl.BlockSpec((tk, 128), col(pairs)), pl.BlockSpec((tk, 128), col(pairs)),
                  pl.BlockSpec((tq, 128), col(0)),
                  pl.BlockSpec((1, 2, tq), lambda j: (j, 0, 0))],
        out_specs=[pl.BlockSpec((tq, 128), col(0)), kblk, kblk, kblk, kblk],
        out_shape=[jax.ShapeDtypeStruct((tq, width), BF16)]
        + [jax.ShapeDtypeStruct((tk, width), F32)] * 4,
        compiler_params=pltpu.CompilerParams(dimension_semantics=('arbitrary',),
                                             vmem_limit_bytes=48 * 1024 * 1024),
        cost_estimate=pl.CostEstimate(flops=flops, bytes_accessed=2 * (2 * tq * width * 2 + 4 * tk * width) + 16 * tk * width,
                                      transcendentals=tq * 2 * tk * (width // HEAD_DIM)),
        name='attn_bwd',
    )(q, kv, kv_s, kv, kv_s, d_ctx, lse)


GELU_C = 0.7978845608028654
GELU_A = 0.044715
BLOCK_F = 1024
SUB_F = 512
ROWS = (slice(0, 256), slice(256, 512))


def mlp_fwd_body(*refs):
    m_ref, h_ref, w1_ref, w2_ref = refs[:4]
    z_ref, g_ref, x_ref, acc_ref = refs[-4:]
    j = pl.program_id(0)

    @pl.when(j == 0)
    def _():
        acc_ref[...] = h_ref[...].astype(F32)

    for i in range(0, BLOCK_F, SUB_F):
        cols = slice(i, i + SUB_F)
        for rows in ROWS:
            z = nt(m_ref[rows, :], w1_ref[cols, :]).astype(BF16)
            z_ref[rows, cols] = z
            zf = z.astype(F32)
            t = jnp.tanh(zf * (GELU_C + (GELU_A * GELU_C) * (zf * zf)))
            half = 0.5 * zf
            g_ref[0, rows, cols] = (half + half * t).astype(BF16)
    for rows in ROWS:
        acc_ref[rows, :] += nn(g_ref[0, rows, :], w2_ref[...])

    @pl.when(j == pl.num_programs(0) - 1)
    def _():
        x_ref[...] = acc_ref[...].astype(BF16)


def mlp_fwd(m, h, w1t, w2, layer, layers, hist):
    t, dim = m.shape
    hidden = w2.shape[0]
    whole = pl.BlockSpec((t, dim), lambda j: (0, 0))
    wblk = pl.BlockSpec((BLOCK_F, dim), lambda j: (j, 0))
    hspec = pl.BlockSpec((1, t, BLOCK_F), lambda j: (layer, 0, j))
    extra = [] if hist is None else [hist]
    return pl.pallas_call(
        mlp_fwd_body,
        grid=(hidden // BLOCK_F,),
        in_specs=[whole, whole, wblk, wblk] + [pl.BlockSpec(memory_space=pl.ANY)] * len(extra),
        out_specs=[pl.BlockSpec((t, BLOCK_F), lambda j: (0, j)), hspec, whole],
        out_shape=[jax.ShapeDtypeStruct((t, hidden), BF16),
                   jax.ShapeDtypeStruct((layers, t, hidden), BF16),
                   jax.ShapeDtypeStruct((t, dim), BF16)],
        scratch_shapes=[pltpu.VMEM((t, dim), F32)],
        input_output_aliases={4: 1} if extra else {},
        compiler_params=pltpu.CompilerParams(dimension_semantics=('arbitrary',), vmem_limit_bytes=48 * 1024 * 1024),
        cost_estimate=pl.CostEstimate(flops=4 * t * dim * hidden, bytes_accessed=4 * dim * hidden + 4 * t * hidden,
                                      transcendentals=t * hidden),
        name='mlp_fwd',
    )(m, h, w1t, w2, *extra)


def mlp_bwd_body(*refs):
    d_ref, h_ref, z_ref, w1_ref, w2_ref = refs[:5]
    up_ref, mid_ref, acc_ref = refs[-3:]
    j = pl.program_id(0)

    @pl.when(j == 0)
    def _():
        acc_ref[...] = jnp.zeros_like(acc_ref)

    for i in range(0, BLOCK_F, SUB_F):
        cols = slice(i, i + SUB_F)
        for rows in ROWS:
            da = nt(d_ref[rows, :], w2_ref[cols, :]).astype(BF16).astype(F32)
            zf = z_ref[rows, cols].astype(F32)
            z2 = zf * zf
            t = jnp.tanh(zf * (GELU_C + (GELU_A * GELU_C) * z2))
            slope = (1.0 + t) * (0.5 + (1.0 - t) * (zf * (0.5 * GELU_C + (1.5 * GELU_A * GELU_C) * z2)))
            up_ref[0, rows, cols] = (da * slope).astype(BF16)
    for rows in ROWS:
        acc_ref[rows, :] += nn(up_ref[0, rows, :], w1_ref[...])

    @pl.when(j == pl.num_programs(0) - 1)
    def _():
        dn = acc_ref[...].astype(BF16).astype(F32)
        hf = h_ref[...].astype(F32)
        inv = lax.rsqrt(jnp.mean(hf * hf, axis=-1, keepdims=True) + EPS_NORM)
        proj = jnp.mean(hf * dn, axis=-1, keepdims=True)
        mid_ref[...] = (d_ref[...].astype(F32) + inv * dn - hf * (inv * inv * inv * proj)).astype(BF16)


def mlp_bwd(d_next, h, z, w1t, w2, layer, layers, hist):
    t, dim = h.shape
    hidden = w2.shape[0]
    whole = pl.BlockSpec((t, dim), lambda j: (0, 0))
    wblk = pl.BlockSpec((BLOCK_F, dim), lambda j: (j, 0))
    hspec = pl.BlockSpec((1, t, BLOCK_F), lambda j: (layer, 0, j))
    extra = [] if hist is None else [hist]
    return pl.pallas_call(
        mlp_bwd_body,
        grid=(hidden // BLOCK_F,),
        in_specs=[whole, whole, pl.BlockSpec((t, BLOCK_F), lambda j: (0, j)), wblk, wblk]
        + [pl.BlockSpec(memory_space=pl.ANY)] * len(extra),
        out_specs=[hspec, whole],
        out_shape=[jax.ShapeDtypeStruct((layers, t, hidden), BF16), jax.ShapeDtypeStruct((t, dim), BF16)],
        scratch_shapes=[pltpu.VMEM((t, dim), F32)],
        input_output_aliases={5: 0} if extra else {},
        compiler_params=pltpu.CompilerParams(dimension_semantics=('arbitrary',), vmem_limit_bytes=48 * 1024 * 1024),
        cost_estimate=pl.CostEstimate(flops=4 * t * dim * hidden, bytes_accessed=4 * dim * hidden + 4 * t * hidden,
                                      transcendentals=t * hidden),
        name='mlp_bwd',
    )(d_next, h, z, w1t, w2, *extra)


BOTH = ('model', 'data')


def solution(mesh):
    spec_col = P(None, 'model')
    spec_row = P('model', None)
    spec_act = P('data', None, None)
    spec_rep = P(None, None)

    def device_step(x_in, cot_out, step_emb, w_q, w_k, w_v, w_o, w_1, w_2):
        layer_count, dim = step_emb.shape
        core = lax.axis_index('data')
        chip = lax.axis_index('model')
        chip_x = lax.rem(chip, 2)
        chip_y = lax.div(chip, 2)

        def take(v, which, axis, parts=2):
            size = v.shape[axis] // parts
            return lax.dynamic_slice_in_dim(v, which * size, size, axis)

        def gather(v):
            return lax.all_gather(v, BOTH, axis=0, tiled=True)

        def scatter(v):
            return lax.psum_scatter(v, BOTH, scatter_dimension=0, tiled=True)

        def my_tokens(v):
            mine = lax.dynamic_index_in_dim(v, chip_x, 0, keepdims=False)
            recv = pp_d(take(mine, 1 - core, 0))
            return jnp.where(core == chip_y, take(mine, core, 0), recv)

        wk = gather(take(w_k, core, 1).T)
        wv = gather(take(w_v, core, 1).T)
        wq = gather(take(w_q, core, 1).T)
        wo = gather(take(w_o, core, 0))
        w1 = gather(take(w_1, core, 1).T)
        w2 = gather(take(w_2, core, 0))

        x_cur = my_tokens(x_in)
        d_cur = my_tokens(cot_out)

        saved = []
        g_hist = None
        for layer in range(layer_count):
            s = x_cur.astype(F32) + step_emb[layer].astype(F32)
            u = rms_norm(s).astype(BF16)
            kv = jnp.concatenate([nt(u, wk).astype(BF16), nt(u, wv).astype(BF16)], axis=1)
            kv_s = pp_d(kv)
            q = nt(u, wq).astype(BF16)
            ctx, lse = attn_fwd(q, kv, kv_s)
            h = (s + nn(ctx, wo)).astype(BF16)
            m = rms_norm(h.astype(F32)).astype(BF16)
            z, g_hist, x_next = mlp_fwd(m, h, w1, w2, layer, layer_count, g_hist)
            saved.append((x_cur, u, q, kv, kv_s, ctx, lse, h, m, z))
            x_cur = x_next

        hist = []
        up_hist = None
        for layer in reversed(range(layer_count)):
            x_l, u, q, kv, kv_s, ctx, lse, h, m, z = saved[layer]
            d_next = d_cur
            if layer == 0:
                next_h = jnp.concatenate([d_next] + [e[0] for e in reversed(hist)], axis=0)
                term_2, d_next = lax.optimization_barrier((tn(g_hist.reshape(-1, g_hist.shape[-1]), next_h), d_next))
                grad_2 = scatter(term_2)
            up_hist, d_mid = mlp_bwd(d_next, h, z, w1, w2, layer, layer_count, up_hist)
            if layer == 0:
                m_h = jnp.concatenate([m] + [e[1] for e in reversed(hist)], axis=0)
                term_1, d_mid = lax.optimization_barrier((tn(up_hist.reshape(-1, up_hist.shape[-1]), m_h), d_mid))
                grad_1 = scatter(term_1)
                mid_h = jnp.concatenate([d_mid] + [e[2] for e in reversed(hist)], axis=0)
                ctx_h = jnp.concatenate([ctx] + [e[3] for e in reversed(hist)], axis=0)
                term_o, d_mid = lax.optimization_barrier((tn(ctx_h, mid_h), d_mid))
                grad_o = scatter(term_o)
            d_ctx = nt(d_mid, wo).astype(BF16)
            dq, dko, dks, dvo, dvs = attn_bwd(q, kv, kv_s, d_ctx, lse)
            dk = (dko + pp_d(dks)).astype(BF16)
            dv = (dvo + pp_d(dvs)).astype(BF16)
            d_norm1 = (nn(dq, wq) + nn(dk, wk) + nn(dv, wv)).astype(BF16)
            s = x_l.astype(F32) + step_emb[layer].astype(F32)
            norm_pull_x = jax.vjp(rms_norm, s)[1]
            d_cur = (d_mid.astype(F32) + norm_pull_x(d_norm1.astype(F32))[0]).astype(BF16)
            hist.append((d_next, m, d_mid, ctx, u, dq, dk, dv))

        u_h, dq_h, dk_h, dv_h = [jnp.concatenate([e[i] for e in reversed(hist)], axis=0) for i in (4, 5, 6, 7)]
        grad_q = scatter(tn(dq_h, u_h))
        grad_k = scatter(tn(dk_h, u_h))
        grad_v = scatter(tn(dv_h, u_h))
        d_x = lax.dynamic_slice_in_dim(gather(d_cur).reshape((4, 1024, dim)), 2 * core, 2, 0)

        def whole(v):
            other = pp_d(v)
            size = v.shape[0]
            out = lax.dynamic_update_slice_in_dim(jnp.zeros((2 * size,) + v.shape[1:], v.dtype), v, core * size, 0)
            return lax.dynamic_update_slice_in_dim(out, other, (1 - core) * size, 0)

        return (whole(grad_q).T, whole(grad_k).T, whole(grad_v).T, whole(grad_o), whole(grad_1).T, whole(grad_2), d_x)

    return jax.shard_map(device_step, mesh=mesh,
                         in_specs=(spec_act, spec_act, spec_rep, spec_col, spec_col, spec_col, spec_row, spec_col, spec_row),
                         out_specs=(spec_col, spec_col, spec_col, spec_row, spec_col, spec_row, spec_act),
                         check_vma=False)
```

time: 2090 us -> 1880 us (0.90)
  matrix products: 728 us -> 301 us
  waiting for transfers between devices: 651 us -> 914 us
  Pallas kernels: 292 us -> 522 us
  other arithmetic: 213 us -> 28.2 us
  starting transfers between devices: 76.6 us -> 5.6 us
  local copies, waits for them, and re-layouts: 113 us -> 86.7 us
    ppermute x50 -> x0, waiting for transfers between devices: 633 us -> none  [the longest x25 377 us: pp_x(): return lax.ppermute(v, 'model', SWAP_X)]
    reduce_scatter x0 -> x6, waiting for transfers between devices: none -> 555 us  [scatter(): return lax.psum_scatter(v, BOTH, scatter_dimension=0, tiled=True)]
    dot_general x103 -> x38, matrix products: 728 us -> 301 us  [dot(): return lax.dot_general(a, b, (dims, ((), ())), preferred_element_type=F32)]
    all_gather x0 -> x7, waiting for transfers between devices: none -> 315 us  [gather(): return lax.all_gather(v, BOTH, axis=0, tiled=True)]
    pallas_call x0 -> x8, Pallas kernels: none -> 230 us  [the longest x4 119 us: mlp_bwd(): pl.pallas_call(mlp_bwd_body, grid=(hidden // BLOCK_F,), in_specs=[whole,...]
    concatenate x18 -> x4, other arithmetic: 88.9 us -> 1.71 us  [device_step(): jnp.concatenate([nt(u, wk).astype(BF16), nt(u, wv).astype(BF16)], axis=1)]
    ppermute x50 -> x0, starting transfers between devices: 59.9 us -> none  [the longest x24 30.6 us: pp_y(): return lax.ppermute(v, 'model', SWAP_Y)]
    add x8 -> x0, other arithmetic: 33.5 us -> none  [the longest x4 17.8 us: reduce_pieces(): own = (a0 + pp_y(a2), b0 + pp_x(b1))]
  transfers between devices with their start and end apart: 129 -> 33, of which waited for: 40 -> 22; matrix products, arithmetic and copies ran while one was open for 21% -> 12% of each run, Pallas kernels for 2% -> 4%
where the time goes in v2:
time: 1880 us; the launch traced here: 1870 us
  waiting for transfers between devices  914 us (49%)
  Pallas kernels  522 us (28%)
  matrix products  301 us (16%)
  local copies, waits for them, and re-layouts  86.7 us (5%)
  other arithmetic  28.2 us (2%)
    reduce_scatter x6, waiting for transfers between devices, scatter(): return lax.psum_scatter(v, BOTH, scatter_dimension=0, tiled=True)  555 us
    all_gather x7, waiting for transfers between devices, gather(): return lax.all_gather(v, BOTH, axis=0, tiled=True)  315 us
    dot_general x38, matrix products, dot(): return lax.dot_general(a, b, (dims, ((), ())), preferred_element_type=F32)  301 us
    pallas_call x4, Pallas kernels, attn_bwd(): pl.pallas_call(attn_bwd_body, grid=(pairs,), in_specs=[pl.BlockSpec((tq,...  197 us
    pallas_call x4, Pallas kernels, mlp_bwd(): pl.pallas_call(mlp_bwd_body, grid=(hidden // BLOCK_F,), in_specs=[whole,...  119 us
    pallas_call x4, Pallas kernels, mlp_fwd(): pl.pallas_call(mlp_fwd_body, grid=(hidden // BLOCK_F,), in_specs=[whole,...  111 us
    pallas_call x4, Pallas kernels, attn_fwd(): pl.pallas_call(attn_fwd_body, grid=(pairs,), in_specs=[pl.BlockSpec((tq,...  95 us
    ppermute x20, waiting for transfers between devices, pp_d(): return lax.ppermute(v, 'data', SWAP_D)  42.4 us
  transfers between devices with their start and end apart: 33, of which 22 were waited for; matrix products, arithmetic and copies ran while one was open for 12% of the time, Pallas kernels for 4%

profile of v2, /device:TPU:0, one launch (start us, length us, event | category | flops | bytes accessed | tf_op | source)
XLA Modules:
  0.0 1873.5 jit_solution(13782640905882613585)
XLA Ops:
  18.8 3.4 constant_dynamic-slice_fusion.1
  32.0 14.9 all-gather.12.cloned.1.call-done
  47.0 6.2 convolution_convert_fusion.13
  53.2 29.4 %all-gather.10.cloned.1.call-done = bf16[1536,1536]{1,0:T(8,128)(2,1)} async-done(((bf16[192,1536]{1,0:T(8,128)(2,1)}), bf16[1536,1536]{1,0:T(8,128)(2,1)}) %all-gather.10.cloned.1.call-update) | async-done | bytes 4718608 | tf_op jit(solution)/shard_map/all_gather | solution.py:300
  82.6 5.1 convolution_convert_fusion.14
  88.4 29.9 %all-gather.8.cloned.1.call-done = bf16[1536,1536]{1,0:T(8,128)(2,1)} async-done(((bf16[192,1536]{1,0:T(8,128)(2,1)}), bf16[1536,1536]{1,0:T(8,128)(2,1)}) %all-gather.8.cloned.1.call-update) | async-done | bytes 4718608 | tf_op jit(solution)/shard_map/all_gather | solution.py:300
  118.3 5.4 convolution_convert_fusion.15.q_ref
  123.7 23.8 %attn_fwd.4 = (bf16[512,1536]{1,0:T(8,128)(2,1)S(1)}, f32[12,2,512]{2,1,0:T(2,128)S(1)}) custom-call(bf16[512,1536]{1,0:T(8,128)(2,1)S(1)} %convolution_convert_fusion.15.q_ref, bf16[512,3072]{1,0:T(8,128)(2,1)} %copy-done.45, bf16[512,3072]{1,0:T(8,128)(2,1)} %collective-permute-done.1.ks_ref.vs_ref, bf16[512,3072]{1,0:T(8,128)(2,1)} %copy-done.45, ...), custom_call_target="tpu_custom_call" | custom-call | flops 12884901888 | bytes 9437184 | tf_op jit(solution)/shard_map/attn_fwd/pallas_call | solution.py:83
  148.7 5.1 all-gather.14.cloned.1.call-done
  153.8 5.6 fusion.59
  159.7 89.4 %all-gather.16.cloned.1.call-done.refs_2_.refs_3_ = bf16[6144,1536]{1,0:T(8,128)(2,1)} async-done(((bf16[768,1536]{1,0:T(8,128)(2,1)}), bf16[6144,1536]{1,0:T(8,128)(2,1)}) %all-gather.16.cloned.1.call-update) | async-done | bytes 18874384 | tf_op jit(solution)/shard_map/all_gather | solution.py:300
  249.1 95.3 %all-gather.18.cloned.1.call-done.refs_3_.refs_4_ = bf16[6144,1536]{1,0:T(8,128)(2,1)} async-done(((bf16[768,1536]{1,0:T(8,128)(2,1)}), bf16[6144,1536]{1,0:T(8,128)(2,1)}) %all-gather.18.cloned.1.call-update) | async-done | bytes 18874384 | tf_op jit(solution)/shard_map/all_gather | solution.py:300
  344.4 27.3 %mlp_fwd.4 = (bf16[512,6144]{1,0:T(8,128)(2,1)}, bf16[4,512,6144]{2,1,0:T(8,128)(2,1)}, bf16[512,1536]{1,0:T(8,128)(2,1)S(1)}) custom-call(bf16[512,1536]{1,0:T(8,128)(2,1)S(1)} %fusion.60.refs_0_, bf16[512,1536]{1,0:T(8,128)(2,1)S(1)} %get-tuple-element.134.refs_1_, bf16[6144,1536]{1,0:T(8,128)(2,1)} %all-gather.16.cloned.1.call-done.refs_2_.refs_3_, ...), custom_call_target="tpu_custom_call" | custom-call | flops 19327352832 | bytes 50331648 | tf_op jit(solution)/shard_map/mlp_fwd/pallas_call | solution.py:209
  372.7 5.8 convolution_convert_fusion.11
  387.5 23.7 %attn_fwd.5 = (bf16[512,1536]{1,0:T(8,128)(2,1)S(1)}, f32[12,2,512]{2,1,0:T(2,128)S(1)}) custom-call(bf16[512,1536]{1,0:T(8,128)(2,1)S(1)} %convolution_convert_fusion.12.q_ref, bf16[512,3072]{1,0:T(8,128)(2,1)} %copy-done.46, bf16[512,3072]{1,0:T(8,128)(2,1)} %collective-permute-done.2.ks_ref.vs_ref, bf16[512,3072]{1,0:T(8,128)(2,1)} %copy-done.46, ...), custom_call_target="tpu_custom_call" | custom-call | flops 12884901888 | bytes 9437184 | tf_op jit(solution)/shard_map/attn_fwd/pallas_call | solution.py:83
  414.3 27.8 %mlp_fwd.5 = (bf16[512,6144]{1,0:T(8,128)(2,1)}, bf16[4,512,6144]{2,1,0:T(8,128)(2,1)}, bf16[512,1536]{1,0:T(8,128)(2,1)S(1)}) custom-call(bf16[512,1536]{1,0:T(8,128)(2,1)S(1)} %fusion.62.refs_0_, bf16[512,1536]{1,0:T(8,128)(2,1)S(1)} %get-tuple-element.136.refs_1_, ...), custom_call_target="tpu_custom_call", output_to_operand_aliasing={{1}: (4, {})} | custom-call | flops 19327352832 | bytes 50331648 | tf_op jit(solution)/shard_map/mlp_fwd/pallas_call | solution.py:209
  443.1 6.3 convolution_convert_fusion.8
  460.0 23.8 %attn_fwd.6 = (bf16[512,1536]{1,0:T(8,128)(2,1)S(1)}, f32[12,2,512]{2,1,0:T(2,128)S(1)}) custom-call(bf16[512,1536]{1,0:T(8,128)(2,1)S(1)} %convolution_convert_fusion.9.q_ref, bf16[512,3072]{1,0:T(8,128)(2,1)} %copy-done.47, bf16[512,3072]{1,0:T(8,128)(2,1)} %copy-done.91, bf16[512,3072]{1,0:T(8,128)(2,1)} %copy-done.47, bf16[512,3072]{1,0:T(8,128)(2,1)} %copy-done.91), custom_call_target="tpu_custom_call" | custom-call | flops 12884901888 | bytes 9437184 | tf_op jit(solution)/shard_map/attn_fwd/pallas_call | solution.py:83
  483.9 5.6 fusion.63
  489.9 27.7 %mlp_fwd.6 = (bf16[512,6144]{1,0:T(8,128)(2,1)}, bf16[4,512,6144]{2,1,0:T(8,128)(2,1)}, bf16[512,1536]{1,0:T(8,128)(2,1)S(1)}) custom-call(bf16[512,1536]{1,0:T(8,128)(2,1)S(1)} %fusion.64.refs_0_, bf16[512,1536]{1,0:T(8,128)(2,1)S(1)} %get-tuple-element.138.refs_1_, ...), custom_call_target="tpu_custom_call", output_to_operand_aliasing={{1}: (4, {})} | custom-call | flops 19327352832 | bytes 50331648 | tf_op jit(solution)/shard_map/mlp_fwd/pallas_call | solution.py:209
  521.2 5.1 convolution_convert_fusion.4
  527.8 7.0 collective-permute-done.5
  539.7 23.7 %attn_fwd.7 = (bf16[512,1536]{1,0:T(8,128)(2,1)S(1)}, f32[12,2,512]{2,1,0:T(2,128)S(1)}) custom-call(bf16[512,1536]{1,0:T(8,128)(2,1)S(1)} %convolution_convert_fusion.6.q_ref, bf16[512,3072]{1,0:T(8,128)(2,1)} %copy-done.48, bf16[512,3072]{1,0:T(8,128)(2,1)} %copy-done.92, bf16[512,3072]{1,0:T(8,128)(2,1)} %copy-done.48, bf16[512,3072]{1,0:T(8,128)(2,1)} %copy-done.92), custom_call_target="tpu_custom_call" | custom-call | flops 12884901888 | bytes 9437184 | tf_op jit(solution)/shard_map/attn_fwd/pallas_call | solution.py:83
  563.5 5.6 fusion.65
  569.4 28.0 %mlp_fwd.7 = (bf16[512,6144]{1,0:T(8,128)(2,1)}, bf16[4,512,6144]{2,1,0:T(8,128)(2,1)}, bf16[512,1536]{1,0:T(8,128)(2,1)}) custom-call(bf16[512,1536]{1,0:T(8,128)(2,1)S(1)} %fusion.66.refs_0_, bf16[512,1536]{1,0:T(8,128)(2,1)S(1)} %get-tuple-element.140.refs_1_, ...), custom_call_target="tpu_custom_call", output_to_operand_aliasing={{1}: (4, {})} | custom-call | flops 19327352832 | bytes 50331648 | tf_op jit(solution)/shard_map/mlp_fwd/pallas_call | solution.py:209
  597.5 29.6 %mlp_bwd.4 = (bf16[4,512,6144]{2,1,0:T(8,128)(2,1)}, bf16[512,1536]{1,0:T(8,128)(2,1)S(1)}) custom-call(bf16[512,1536]{1,0:T(8,128)(2,1)S(1)} %bitcast_select_fusion.refs_0_, bf16[512,1536]{1,0:T(8,128)(2,1)S(1)} %get-tuple-element.140.refs_1_, bf16[512,6144]{1,0:T(8,128)(2,1)} %get-tuple-element.71.refs_2_, ...), custom_call_target="tpu_custom_call" | custom-call | flops 19327352832 | bytes 50331648 | tf_op jit(solution)/shard_map/mlp_bwd/pallas_call | solution.py:263
  627.1 5.5 convolution_convert_fusion.3.do_ref
  632.6 49.3 %attn_bwd.4 = (bf16[512,1536]{1,0:T(8,128)(2,1)S(1)}, f32[512,1536]{1,0:T(8,128)}, f32[512,1536]{1,0:T(8,128)}, f32[512,1536]{1,0:T(8,128)}, f32[512,1536]{1,0:T(8,128)}) custom-call(bf16[512,1536]{1,0:T(8,128)(2,1)S(1)} %convolution_convert_fusion.6.q_ref, bf16[512,3072]{1,0:T(8,128)(2,1)} %copy-done.48, bf16[512,3072]{1,0:T(8,128)(2,1)} %copy-done.92, ...), custom_call_target="tpu_custom_call" | custom-call | flops 32212254720 | bytes 25165824 | tf_op jit(solution)/shard_map/attn_bwd/pallas_call | solution.py:150
  682.5 5.4 collective-permute-done.6
  690.4 5.1 fusion.97
  702.7 29.8 %mlp_bwd.5 = (bf16[4,512,6144]{2,1,0:T(8,128)(2,1)}, bf16[512,1536]{1,0:T(8,128)(2,1)S(1)}) custom-call(bf16[512,1536]{1,0:T(8,128)(2,1)S(1)} %fusion.72.refs_0_, bf16[512,1536]{1,0:T(8,128)(2,1)S(1)} %get-tuple-element.138.refs_1_, bf16[512,6144]{1,0:T(8,128)(2,1)} %get-tuple-element.79.refs_2_, ...), custom_call_target="tpu_custom_call", output_to_operand_aliasing={{0}: (5, {})} | custom-call | flops 19327352832 | bytes 50331648 | tf_op jit(solution)/shard_map/mlp_bwd/pallas_call | solution.py:263
  732.5 5.6 convolution_convert_fusion.2.do_ref
  738.1 49.1 %attn_bwd.5 = (bf16[512,1536]{1,0:T(8,128)(2,1)S(1)}, f32[512,1536]{1,0:T(8,128)}, f32[512,1536]{1,0:T(8,128)}, f32[512,1536]{1,0:T(8,128)}, f32[512,1536]{1,0:T(8,128)}) custom-call(bf16[512,1536]{1,0:T(8,128)(2,1)S(1)} %copy-done.37, bf16[512,3072]{1,0:T(8,128)(2,1)} %copy-done.47, bf16[512,3072]{1,0:T(8,128)(2,1)} %copy-done.91, ...), custom_call_target="tpu_custom_call" | custom-call | flops 32212254720 | bytes 25165824 | tf_op jit(solution)/shard_map/attn_bwd/pallas_call | solution.py:150
  787.8 5.4 collective-permute-done.8
  806.1 29.9 %mlp_bwd.6 = (bf16[4,512,6144]{2,1,0:T(8,128)(2,1)}, bf16[512,1536]{1,0:T(8,128)(2,1)S(1)}) custom-call(bf16[512,1536]{1,0:T(8,128)(2,1)S(1)} %fusion.74.refs_0_, bf16[512,1536]{1,0:T(8,128)(2,1)S(1)} %copy-done.7, bf16[512,6144]{1,0:T(8,128)(2,1)} %get-tuple-element.88.refs_2_, ...), custom_call_target="tpu_custom_call", output_to_operand_aliasing={{0}: (5, {})} | custom-call | flops 19327352832 | bytes 50331648 | tf_op jit(solution)/shard_map/mlp_bwd/pallas_call | solution.py:263
  836.0 5.6 convolution_convert_fusion.1.do_ref
  841.6 49.1 %attn_bwd.6 = (bf16[512,1536]{1,0:T(8,128)(2,1)S(1)}, f32[512,1536]{1,0:T(8,128)}, f32[512,1536]{1,0:T(8,128)}, f32[512,1536]{1,0:T(8,128)}, f32[512,1536]{1,0:T(8,128)}) custom-call(bf16[512,1536]{1,0:T(8,128)(2,1)S(1)} %copy-done.35, bf16[512,3072]{1,0:T(8,128)(2,1)} %copy-done.46, bf16[512,3072]{1,0:T(8,128)(2,1)} %collective-permute-done.2.ks_ref.vs_ref, ...), custom_call_target="tpu_custom_call" | custom-call | flops 32212254720 | bytes 25165824 | tf_op jit(solution)/shard_map/attn_bwd/pallas_call | solution.py:150
  891.3 5.4 collective-permute-done.10
  899.1 5.2 fusion.101
  912.2 45.4 %fusion.8 = f32[6144,1536]{1,0:T(8,128)} fusion(bf16[2048,6144]{1,0:T(8,128)(2,1)} %bitcast.130, bf16[512,1536]{1,0:T(8,128)(2,1)S(1)} %copy-done.19, bf16[512,1536]{1,0:T(8,128)(2,1)S(1)} %fusion.72.refs_0_, bf16[512,1536]{1,0:T(8,128)(2,1)S(1)} %fusion.74.refs_0_, bf16[512,1536]{1,0:T(8,128)(2,1)S(1)} %fusion.76.refs_0_), kind=kOutput, calls=%fused_computation.8 | convolution fusion | flops 38679871488 | bytes 69206016 | tf_op jit(solution)/shard_map/dot_general | solution.py:28
  957.6 29.9 %mlp_bwd.7 = (bf16[4,512,6144]{2,1,0:T(8,128)(2,1)}, bf16[512,1536]{1,0:T(8,128)(2,1)S(1)}) custom-call(bf16[512,1536]{1,0:T(8,128)(2,1)S(1)} %fusion.76.refs_0_, bf16[512,1536]{1,0:T(8,128)(2,1)S(1)} %get-tuple-element.134.refs_1_, bf16[512,6144]{1,0:T(8,128)(2,1)} %get-tuple-element.98.refs_2_, ...), custom_call_target="tpu_custom_call", output_to_operand_aliasing={{0}: (5, {})} | custom-call | flops 19327352832 | bytes 50331648 | tf_op jit(solution)/shard_map/mlp_bwd/pallas_call | solution.py:263
  988.8 45.3 %fusion.16 = f32[6144,1536]{1,0:T(8,128)} fusion(bf16[2048,6144]{1,0:T(8,128)(2,1)} %bitcast.86, bf16[512,1536]{1,0:T(8,128)(2,1)S(1)} %copy-done.17, bf16[512,1536]{1,0:T(8,128)(2,1)S(1)} %copy-done.13, bf16[512,1536]{1,0:T(8,128)(2,1)S(1)} %copy-done.11, bf16[512,1536]{1,0:T(8,128)(2,1)S(1)} %copy-done.9), kind=kOutput, calls=%fused_computation.16 | convolution fusion | flops 38679871488 | bytes 69206016 | tf_op jit(solution)/shard_map/dot_general | solution.py:28
  1036.0 20.3 %fusion = f32[1536,1536]{1,0:T(8,128)} fusion(bf16[512,1536]{1,0:T(8,128)(2,1)} %copy-done.41, bf16[512,1536]{1,0:T(8,128)(2,1)} %copy-done.40, bf16[512,1536]{1,0:T(8,128)(2,1)} %copy-done.39, bf16[512,1536]{1,0:T(8,128)(2,1)} %copy-done.38, bf16[512,1536]{1,0:T(8,128)(2,1)S(1)} %copy-done.15, bf16[512,1536]{1,0:T(8,128)(2,1)S(1)} %copy-done.21, ...), kind=kOutput, calls=%fused_computation | convolution fusion | flops 9714008064 | bytes 22020096 | tf_op jit(solution)/shard_map/dot_general | solution.py:28
  1056.3 6.8 convolution_convert_fusion.do_ref
  1063.1 49.9 %attn_bwd.7 = (bf16[512,1536]{1,0:T(8,128)(2,1)S(1)}, f32[512,1536]{1,0:T(8,128)}, f32[512,1536]{1,0:T(8,128)}, f32[512,1536]{1,0:T(8,128)}, f32[512,1536]{1,0:T(8,128)}) custom-call(bf16[512,1536]{1,0:T(8,128)(2,1)S(1)} %copy-done.33, bf16[512,3072]{1,0:T(8,128)(2,1)} %copy-done.45, bf16[512,3072]{1,0:T(8,128)(2,1)} %collective-permute-done.1.ks_ref.vs_ref, ...), custom_call_target="tpu_custom_call" | custom-call | flops 32212254720 | bytes 25165824 | tf_op jit(solution)/shard_map/attn_bwd/pallas_call | solution.py:150
  1114.1 17.8 fusion.31
  1133.1 5.6 collective-permute-done.15
  1140.3 18.9 %fusion.47 = f32[1536,1536]{1,0:T(8,128)} fusion(bf16[512,1536]{1,0:T(8,128)(2,1)} %copy-done.60, bf16[512,1536]{1,0:T(8,128)(2,1)} %copy-done.62, bf16[512,1536]{1,0:T(8,128)(2,1)} %copy-done.64, bf16[512,1536]{1,0:T(8,128)(2,1)} %add_convert_fusion, bf16[512,1536]{1,0:T(8,128)(2,1)} %copy-done.57, bf16[512,1536]{1,0:T(8,128)(2,1)} %copy-done.56, ...), kind=kOutput, calls=%fused_computation.48 | convolution fusion | flops 9714008064 | bytes 22020096 | tf_op jit(solution)/shard_map/dot_general | solution.py:28
  1159.8 5.8 collective-permute-done.13
  1167.1 18.7 fusion.39
  1187.3 4.7 fusion.104
  1192.0 4.6 fusion.103
  1201.9 49.7 %reduce-scatter.15.cloned.1.call-done = f32[768,1536]{1,0:T(8,128)} async-done(((f32[6144,1536]{1,0:T(8,128)}), f32[768,1536]{1,0:T(8,128)}) %reduce-scatter.15.cloned.1.call-update) | async-done | bytes 4718608 | tf_op jit(solution)/shard_map/reduce_scatter | solution.py:303
  1251.6 220.9 %reduce-scatter.17.cloned.1.call-done = f32[768,1536]{1,0:T(8,128)} async-done(((f32[6144,1536]{1,0:T(8,128)}), f32[768,1536]{1,0:T(8,128)}) %reduce-scatter.17.cloned.1.call-update) | async-done | bytes 4718608 | tf_op jit(solution)/shard_map/reduce_scatter | solution.py:303
  1472.5 72.5 %reduce-scatter.7.cloned.1.call-done = f32[192,1536]{1,0:T(8,128)} async-done(((f32[1536,1536]{1,0:T(8,128)}), f32[192,1536]{1,0:T(8,128)}) %reduce-scatter.7.cloned.1.call-update) | async-done | bytes 1179664 | tf_op jit(solution)/shard_map/reduce_scatter | solution.py:303
  1545.0 71.8 %reduce-scatter.13.cloned.1.call-done = f32[192,1536]{1,0:T(8,128)} async-done(((f32[1536,1536]{1,0:T(8,128)}), f32[192,1536]{1,0:T(8,128)}) %reduce-scatter.13.cloned.1.call-update) | async-done | bytes 1179664 | tf_op jit(solution)/shard_map/reduce_scatter | solution.py:303
  1619.6 69.1 %reduce-scatter.11.cloned.1.call-done = f32[192,1536]{1,0:T(8,128)} async-done(((f32[1536,1536]{1,0:T(8,128)}), f32[192,1536]{1,0:T(8,128)}) %reduce-scatter.11.cloned.1.call-update) | async-done | bytes 1179664 | tf_op jit(solution)/shard_map/reduce_scatter | solution.py:303
  1690.4 70.7 %reduce-scatter.9.cloned.1.call-done = f32[192,1536]{1,0:T(8,128)} async-done(((f32[1536,1536]{1,0:T(8,128)}), f32[192,1536]{1,0:T(8,128)}) %reduce-scatter.9.cloned.1.call-update) | async-done | bytes 1179664 | tf_op jit(solution)/shard_map/reduce_scatter | solution.py:303
  1779.1 50.9 %all-gather.20.cloned.1.call-done = bf16[4096,1536]{1,0:T(8,128)(2,1)} async-done(((bf16[512,1536]{1,0:T(8,128)(2,1)}), bf16[4096,1536]{1,0:T(8,128)(2,1)}) %all-gather.20.cloned.1.call-update) | async-done | bytes 12582928 | tf_op jit(solution)/shard_map/all_gather | solution.py:300
  1830.0 6.1 constant_dynamic-slice_fusion
  1837.9 4.9 broadcast.152.clone
  1847.3 4.9 constant_dynamic-update-slice_fusion.2
  1852.2 9.7 copy.34
  1861.9 4.8 constant_dynamic-update-slice_fusion
  (421 shorter events, 136.7 us)
Async XLA Ops:
  7.2 39.8 %all-gather.12.cloned.1.call-start = ((), (), s32[]{:S(2)}) async-start(), calls=%async_computation.8 | async-start | bytes 5308416 | tf_op jit(solution)/shard_map/all_gather | solution.py:300
  10.8 71.8 %all-gather.10.cloned.1.call-start = ((), (), s32[]{:S(2)}) async-start(), calls=%async_computation.7 | async-start | bytes 5308416 | tf_op jit(solution)/shard_map/all_gather | solution.py:300
  12.0 106.3 %all-gather.8.cloned.1.call-start = ((), (), s32[]{:S(2)}) async-start(), calls=%async_computation.6 | async-start | bytes 5308416 | tf_op jit(solution)/shard_map/all_gather | solution.py:300
  13.5 140.3 %all-gather.14.cloned.1.call-start = ((), (), s32[]{:S(2)}) async-start(), calls=%async_computation.9 | async-start | bytes 5308416 | tf_op jit(solution)/shard_map/all_gather | solution.py:300
  14.4 234.7 %all-gather.16.cloned.1.call-start = ((), (), s32[]{:S(2)}) async-start(), calls=%async_computation.10 | async-start | bytes 21233664 | tf_op jit(solution)/shard_map/all_gather | solution.py:300
  18.7 325.6 %all-gather.18.cloned.1.call-start = ((), (), s32[]{:S(2)}) async-start(), calls=%async_computation.11 | async-start | bytes 21233664 | tf_op jit(solution)/shard_map/all_gather | solution.py:300
  22.2 1229.4 %reduce-scatter.15.cloned.1.call-start = ((), (), s32[]{:S(2)}) async-start(), calls=%async_computation.16 | async-start | bytes 42467328 | tf_op jit(solution)/shard_map/reduce_scatter | solution.py:303
  24.1 3.6 collective-permute-start
  25.2 128.5 %copy-start.71 = (f32[1536]{0:T(1024)}, f32[1536]{0:T(1024)S(1)}, u32[]{:S(2)}) copy-start(f32[1536]{0:T(1024)S(1)} %get-tuple-element.129) | copy-start | bytes 18436
  25.2 385.9 %copy-start.73 = (f32[1536]{0:T(1024)}, f32[1536]{0:T(1024)S(1)}, u32[]{:S(2)}) copy-start(f32[1536]{0:T(1024)S(1)} %get-tuple-element.128) | copy-start | bytes 18436
  25.3 458.6 %copy-start.75 = (f32[1536]{0:T(1024)}, f32[1536]{0:T(1024)S(1)}, u32[]{:S(2)}) copy-start(f32[1536]{0:T(1024)S(1)} %get-tuple-element.130) | copy-start | bytes 18436
  32.0 50.6 %copy-start.54 = (bf16[512,1536]{1,0:T(8,128)(2,1)}, bf16[512,1536]{1,0:T(8,128)(2,1)S(1)}, u32[]{:S(2)}) copy-start(bf16[512,1536]{1,0:T(8,128)(2,1)S(1)} %multiply_convert_fusion.3) | copy-start | bytes 4718596
  88.1 35.6 %copy-start.45 = (bf16[512,3072]{1,0:T(8,128)(2,1)}, bf16[512,3072]{1,0:T(8,128)(2,1)S(1)}, u32[]{:S(2)}) copy-start(bf16[512,3072]{1,0:T(8,128)(2,1)S(1)} %pad_maximum_fusion.1.ko_ref.vo_ref) | copy-start | bytes 9437188
  88.1 35.6 %collective-permute-start.1 = (bf16[512,3072]{1,0:T(8,128)(2,1)S(1)}, bf16[512,3072]{1,0:T(8,128)(2,1)}, u32[]{:S(2)}, u32[]{:S(2)}) collective-permute-start(bf16[512,3072]{1,0:T(8,128)(2,1)S(1)} %pad_maximum_fusion.1.ko_ref.vo_ref), channel_id=1, source_target_pairs={{0,1},{1,0},{2,3},{3,2},{4,5},{5,4},{6,7},{7,6}} | collective-permute-start | bytes 9437192 | tf_op jit(solution)/shard_map/ppermute | solution.py:20
  159.7 212.0 %copy-start.8 = (bf16[512,1536]{1,0:T(8,128)(2,1)}, bf16[512,1536]{1,0:T(8,128)(2,1)S(1)}, u32[]{:S(2)}) copy-start(bf16[512,1536]{1,0:T(8,128)(2,1)S(1)} %fusion.60.refs_0_) | copy-start | bytes 4718596
  371.7 39.5 %copy-start.2 = (bf16[512,1536]{1,0:T(8,128)(2,1)}, bf16[512,1536]{1,0:T(8,128)(2,1)S(1)}, u32[]{:S(2)}) copy-start(bf16[512,1536]{1,0:T(8,128)(2,1)S(1)} %get-tuple-element.61) | copy-start | bytes 4718596
  381.7 5.8 collective-permute-start.2
  381.9 29.3 %slice-start.34 = ((s8[4718592]{0:T(1024)(128)(4,1)}), s8[4194304]{0:T(1024)(128)(4,1)S(1)}, s32[]{:S(2)}) async-start(s8[4718592]{0:T(1024)(128)(4,1)} %bitcast.128), calls=%async_computation.53 | async-start | bytes 8388608
  384.6 26.6 %slice-start.35 = ((s8[4718592]{0:T(1024)(128)(4,1)}), s8[524288]{0:T(1024)(128)(4,1)S(1)}, s32[]{:S(2)}) async-start(s8[4718592]{0:T(1024)(128)(4,1)} %bitcast.128), calls=%async_computation.54 | async-start | bytes 1048576
  414.0 28.1 %copy-start.6 = (bf16[512,1536]{1,0:T(8,128)(2,1)}, bf16[512,1536]{1,0:T(8,128)(2,1)S(1)}, u32[]{:S(2)}) copy-start(bf16[512,1536]{1,0:T(8,128)(2,1)S(1)} %get-tuple-element.136.refs_1_) | copy-start | bytes 4718596
  414.3 27.8 %copy-start.10 = (bf16[512,1536]{1,0:T(8,128)(2,1)}, bf16[512,1536]{1,0:T(8,128)(2,1)S(1)}, u32[]{:S(2)}) copy-start(bf16[512,1536]{1,0:T(8,128)(2,1)S(1)} %fusion.62.refs_0_) | copy-start | bytes 4718596
  442.1 41.8 %copy-start.4 = (bf16[512,1536]{1,0:T(8,128)(2,1)}, bf16[512,1536]{1,0:T(8,128)(2,1)S(1)}, u32[]{:S(2)}) copy-start(bf16[512,1536]{1,0:T(8,128)(2,1)S(1)} %get-tuple-element.64) | copy-start | bytes 4718596
  452.6 5.7 collective-permute-start.3
  455.5 28.3 %copy-start.36 = (bf16[512,1536]{1,0:T(8,128)(2,1)}, bf16[512,1536]{1,0:T(8,128)(2,1)S(1)}, u32[]{:S(2)}) copy-start(bf16[512,1536]{1,0:T(8,128)(2,1)S(1)} %convolution_convert_fusion.9.q_ref) | copy-start | bytes 4718596
  489.9 27.7 %copy-start.12 = (bf16[512,1536]{1,0:T(8,128)(2,1)}, bf16[512,1536]{1,0:T(8,128)(2,1)S(1)}, u32[]{:S(2)}) copy-start(bf16[512,1536]{1,0:T(8,128)(2,1)S(1)} %fusion.64.refs_0_) | copy-start | bytes 4718596
  489.9 28.6 %slice-start.16 = ((s8[4718592]{0:T(1024)(128)(4,1)}), s8[4194304]{0:T(1024)(128)(4,1)S(1)}, s32[]{:S(2)}) async-start(s8[4718592]{0:T(1024)(128)(4,1)} %bitcast.110), calls=%async_computation.35 | async-start | bytes 8388608
  489.9 27.7 %copy-start.77 = (f32[1536]{0:T(1024)S(1)}, f32[1536]{0:T(1024)}, u32[]{:S(2)}) copy-start(f32[1536]{0:T(1024)} %get-tuple-element.127) | copy-start | bytes 18436
  489.9 28.6 %slice-start.17 = ((s8[4718592]{0:T(1024)(128)(4,1)}), s8[524288]{0:T(1024)(128)(4,1)S(1)}, s32[]{:S(2)}) async-start(s8[4718592]{0:T(1024)(128)(4,1)} %bitcast.110), calls=%async_computation.36 | async-start | bytes 1048576
  526.9 11.2 collective-permute-start.4
  527.5 7.3 collective-permute-start.5
  535.4 62.0 %copy-start.18 = (bf16[512,1536]{1,0:T(8,128)(2,1)}, bf16[512,1536]{1,0:T(8,128)(2,1)S(1)}, u32[]{:S(2)}) copy-start(bf16[512,1536]{1,0:T(8,128)(2,1)S(1)} %bitcast_select_fusion.refs_0_) | copy-start | bytes 4718596
  569.4 28.0 %copy-start.16 = (bf16[512,1536]{1,0:T(8,128)(2,1)}, bf16[512,1536]{1,0:T(8,128)(2,1)S(1)}, u32[]{:S(2)}) copy-start(bf16[512,1536]{1,0:T(8,128)(2,1)S(1)} %fusion.66.refs_0_) | copy-start | bytes 4718596
  627.1 74.6 %copy-start.14 = (bf16[512,1536]{1,0:T(8,128)(2,1)}, bf16[512,1536]{1,0:T(8,128)(2,1)S(1)}, u32[]{:S(2)}) copy-start(bf16[512,1536]{1,0:T(8,128)(2,1)S(1)} %get-tuple-element.72) | copy-start | bytes 4718596
  682.0 5.9 collective-permute-start.6
  682.2 13.3 collective-permute-start.7
  732.5 72.2 %copy-start.20 = (bf16[512,1536]{1,0:T(8,128)(2,1)}, bf16[512,1536]{1,0:T(8,128)(2,1)S(1)}, u32[]{:S(2)}) copy-start(bf16[512,1536]{1,0:T(8,128)(2,1)S(1)} %get-tuple-element.81) | copy-start | bytes 4718596
  732.5 63.1 %slice-start.18 = ((s8[4718592]{0:T(1024)(128)(4,1)}), s8[4194304]{0:T(1024)(128)(4,1)S(1)}, s32[]{:S(2)}) async-start(s8[4718592]{0:T(1024)(128)(4,1)} %bitcast.112), calls=%async_computation.37 | async-start | bytes 8388608
  738.1 57.5 %slice-start.19 = ((s8[4718592]{0:T(1024)(128)(4,1)}), s8[524288]{0:T(1024)(128)(4,1)S(1)}, s32[]{:S(2)}) async-start(s8[4718592]{0:T(1024)(128)(4,1)} %bitcast.112), calls=%async_computation.38 | async-start | bytes 1048576
  787.2 5.9 collective-permute-start.8
  787.5 10.8 collective-permute-start.9
  836.0 74.8 %copy-start.24 = (bf16[512,1536]{1,0:T(8,128)(2,1)}, bf16[512,1536]{1,0:T(8,128)(2,1)S(1)}, u32[]{:S(2)}) copy-start(bf16[512,1536]{1,0:T(8,128)(2,1)S(1)} %get-tuple-element.90) | copy-start | bytes 4718596
  890.7 5.9 collective-permute-start.10
  891.0 13.4 collective-permute-start.11
  957.6 31.1 %copy-start.9 = (bf16[512,1536]{1,0:T(8,128)(2,1)S(1)}, bf16[512,1536]{1,0:T(8,128)(2,1)}, u32[]{:S(2)}) copy-start(bf16[512,1536]{1,0:T(8,128)(2,1)} %copy-done.8) | copy-start | bytes 4718596
  957.6 31.1 %copy-start.11 = (bf16[512,1536]{1,0:T(8,128)(2,1)S(1)}, bf16[512,1536]{1,0:T(8,128)(2,1)}, u32[]{:S(2)}) copy-start(bf16[512,1536]{1,0:T(8,128)(2,1)} %copy-done.10) | copy-start | bytes 4718596
  957.6 31.1 %copy-start.13 = (bf16[512,1536]{1,0:T(8,128)(2,1)S(1)}, bf16[512,1536]{1,0:T(8,128)(2,1)}, u32[]{:S(2)}) copy-start(bf16[512,1536]{1,0:T(8,128)(2,1)} %copy-done.12) | copy-start | bytes 4718596
  957.6 31.1 %copy-start.17 = (bf16[512,1536]{1,0:T(8,128)(2,1)S(1)}, bf16[512,1536]{1,0:T(8,128)(2,1)}, u32[]{:S(2)}) copy-start(bf16[512,1536]{1,0:T(8,128)(2,1)} %copy-done.16) | copy-start | bytes 4718596
  1034.1 438.4 %reduce-scatter.17.cloned.1.call-start = ((), (), s32[]{:S(2)}) async-start(), calls=%async_computation.17 | async-start | bytes 42467328 | tf_op jit(solution)/shard_map/reduce_scatter | solution.py:303
  1034.9 510.1 %reduce-scatter.7.cloned.1.call-start = ((), (), s32[]{:S(2)}) async-start(), calls=%async_computation.12 | async-start | bytes 10616832 | tf_op jit(solution)/shard_map/reduce_scatter | solution.py:303
  1063.1 51.0 %copy-start.26 = (bf16[512,1536]{1,0:T(8,128)(2,1)S(1)}, bf16[512,1536]{1,0:T(8,128)(2,1)}, u32[]{:S(2)}) copy-start(bf16[512,1536]{1,0:T(8,128)(2,1)} %copy-done.25) | copy-start | bytes 4718596
  1063.1 51.0 %copy-start.28 = (bf16[512,1536]{1,0:T(8,128)(2,1)S(1)}, bf16[512,1536]{1,0:T(8,128)(2,1)}, u32[]{:S(2)}) copy-start(bf16[512,1536]{1,0:T(8,128)(2,1)} %copy-done.27) | copy-start | bytes 4718596
  1132.0 484.8 %reduce-scatter.13.cloned.1.call-start = ((), (), s32[]{:S(2)}) async-start(), calls=%async_computation.15 | async-start | bytes 10616832 | tf_op jit(solution)/shard_map/reduce_scatter | solution.py:303
  1132.6 556.2 %reduce-scatter.11.cloned.1.call-start = ((), (), s32[]{:S(2)}) async-start(), calls=%async_computation.14 | async-start | bytes 10616832 | tf_op jit(solution)/shard_map/reduce_scatter | solution.py:303
  1132.8 5.9 collective-permute-start.15
  1159.2 601.9 %reduce-scatter.9.cloned.1.call-start = ((), (), s32[]{:S(2)}) async-start(), calls=%async_computation.13 | async-start | bytes 10616832 | tf_op jit(solution)/shard_map/reduce_scatter | solution.py:303
  1159.7 5.9 collective-permute-start.13
  1185.9 644.1 %all-gather.20.cloned.1.call-start = ((), (), s32[]{:S(2)}) async-start(), calls=%async_computation.18 | async-start | bytes 14155776 | tf_op jit(solution)/shard_map/all_gather | solution.py:300
  1251.6 595.7 %collective-permute-start.18 = (f32[768,1536]{1,0:T(8,128)}, f32[768,1536]{1,0:T(8,128)}, u32[]{:S(2)}, u32[]{:S(2)}) collective-permute-start(f32[768,1536]{1,0:T(8,128)} %reduce-scatter.15.cloned.1.call-done), channel_id=1, source_target_pairs={{0,1},{1,0},{2,3},{3,2},{4,5},{5,4},{6,7},{7,6}} | collective-permute-start | bytes 14155784 | tf_op jit(solution)/shard_map/ppermute | solution.py:20
  1472.5 389.4 %collective-permute-start.19 = (f32[768,1536]{1,0:T(8,128)}, f32[768,1536]{1,0:T(8,128)}, u32[]{:S(2)}, u32[]{:S(2)}) collective-permute-start(f32[768,1536]{1,0:T(8,128)} %reduce-scatter.17.cloned.1.call-done), channel_id=1, source_target_pairs={{0,1},{1,0},{2,3},{3,2},{4,5},{5,4},{6,7},{7,6}} | collective-permute-start | bytes 14155784 | tf_op jit(solution)/shard_map/ppermute | solution.py:20
  1545.0 145.4 %collective-permute-start.12 = (f32[192,1536]{1,0:T(8,128)}, f32[192,1536]{1,0:T(8,128)}, u32[]{:S(2)}, u32[]{:S(2)}) collective-permute-start(f32[192,1536]{1,0:T(8,128)} %reduce-scatter.7.cloned.1.call-done), channel_id=1, source_target_pairs={{0,1},{1,0},{2,3},{3,2},{4,5},{5,4},{6,7},{7,6}} | collective-permute-start | bytes 3538952 | tf_op jit(solution)/shard_map/ppermute | solution.py:20
  1616.8 147.6 %collective-permute-start.17 = (f32[192,1536]{1,0:T(8,128)}, f32[192,1536]{1,0:T(8,128)}, u32[]{:S(2)}, u32[]{:S(2)}) collective-permute-start(f32[192,1536]{1,0:T(8,128)} %reduce-scatter.13.cloned.1.call-done), channel_id=1, source_target_pairs={{0,1},{1,0},{2,3},{3,2},{4,5},{5,4},{6,7},{7,6}} | collective-permute-start | bytes 3538952 | tf_op jit(solution)/shard_map/ppermute | solution.py:20
  1688.7 81.4 %collective-permute-start.16 = (f32[192,1536]{1,0:T(8,128)}, f32[192,1536]{1,0:T(8,128)}, u32[]{:S(2)}, u32[]{:S(2)}) collective-permute-start(f32[192,1536]{1,0:T(8,128)} %reduce-scatter.11.cloned.1.call-done), channel_id=1, source_target_pairs={{0,1},{1,0},{2,3},{3,2},{4,5},{5,4},{6,7},{7,6}} | collective-permute-start | bytes 3538952 | tf_op jit(solution)/shard_map/ppermute | solution.py:20
  1761.1 14.7 collective-permute-start.14
  1777.1 60.1 %slice-start = ((s8[4718592]{0:T(1024)(128)(4,1)}), s8[524288]{0:T(1024)(128)(4,1)S(1)}, s32[]{:S(2)}) async-start(s8[4718592]{0:T(1024)(128)(4,1)} %bitcast.90), calls=%async_computation.19 | async-start | bytes 1048576
  (98 other events, 575.3 us)
Sparse Core Ops, SparseCore 0:
  10.9 36.0 all-gather.11
  49.4 33.2 all-gather.9
  85.0 33.2 all-gather.7
  120.5 33.2 all-gather.13
  156.0 93.0 all-gather.15
  251.3 93.0 all-gather.17
  1034.2 217.3 reduce-scatter.14
  1255.1 217.3 reduce-scatter.16
  1476.5 68.4 reduce-scatter.6
  1548.3 68.4 reduce-scatter.12
  1620.2 68.4 reduce-scatter.10
  1692.6 68.4 reduce-scatter.8
  1763.5 66.4 all-gather.19

commit v3 on v2

--- a/solution.py
+++ b/solution.py
@@ -14,6 +14,18 @@
 SCALE = HEAD_DIM ** -0.5
 
 SWAP_D = [(0, 1), (1, 0)]
+
+
+SWAP_X = [(0, 1), (1, 0), (2, 3), (3, 2)]
+SWAP_Y = [(0, 2), (2, 0), (1, 3), (3, 1)]
+
+
+def pp_x(v):
+    return lax.ppermute(v, 'model', SWAP_X)
+
+
+def pp_y(v):
+    return lax.ppermute(v, 'model', SWAP_Y)
 
 
 def pp_d(v):
@@ -98,8 +110,9 @@
     )(q, kv, kv_s, kv, kv_s)
 
 
-def attn_bwd_body(q_ref, ko_ref, ks_ref, vo_ref, vs_ref, do_ref, lse_ref,
-                  dq_ref, dko_ref, dks_ref, dvo_ref, dvs_ref):
+def attn_bwd_body(*refs):
+    q_ref, ko_ref, ks_ref, vo_ref, vs_ref, do_ref, lse_ref = refs[:7]
+    dq_ref, dko_ref, dks_ref, dvo_ref, dvs_ref = refs[-5:]
     tk = ko_ref.shape[0]
     k = jnp.concatenate([ko_ref[...], ks_ref[...]], axis=0)
     v = jnp.concatenate([vo_ref[...], vs_ref[...]], axis=0)
@@ -131,13 +144,13 @@
             dko_ref[...] += dk[:tk]
             dks_ref[...] += dk[tk:]
             dqs.append(tn(k, ds)[h * HEAD_DIM:(h + 1) * HEAD_DIM, :] * SCALE)
-        dq_ref[rows, :] = jnp.concatenate(dqs, axis=0).T.astype(BF16)
+        dq_ref[0, rows, :] = jnp.concatenate(dqs, axis=0).T.astype(BF16)
         return carry
 
     lax.fori_loop(0, tq // chunk, step, 0)
 
 
-def attn_bwd(q, kv, kv_s, d_ctx, lse):
+def attn_bwd(q, kv, kv_s, d_ctx, lse, layer, layers, hist):
     tq, width = q.shape
     tk = kv.shape[0]
     pairs = width // 128
@@ -147,6 +160,7 @@
 
     flops = 5 * 2 * tq * (2 * tk) * 256 * (width // HEAD_DIM)
     kblk = pl.BlockSpec((tk, 128), col(0))
+    extra = [] if hist is None else [hist]
     return pl.pallas_call(
         attn_bwd_body,
         grid=(pairs,),
@@ -154,16 +168,18 @@
                   kblk, kblk,
                   pl.BlockSpec((tk, 128), col(pairs)), pl.BlockSpec((tk, 128), col(pairs)),
                   pl.BlockSpec((tq, 128), col(0)),
-                  pl.BlockSpec((1, 2, tq), lambda j: (j, 0, 0))],
-        out_specs=[pl.BlockSpec((tq, 128), col(0)), kblk, kblk, kblk, kblk],
-        out_shape=[jax.ShapeDtypeStruct((tq, width), BF16)]
+                  pl.BlockSpec((1, 2, tq), lambda j: (j, 0, 0))]
+        + [pl.BlockSpec(memory_space=pl.ANY)] * len(extra),
+        out_specs=[pl.BlockSpec((1, tq, 128), lambda j: (layer, 0, j)), kblk, kblk, kblk, kblk],
+        out_shape=[jax.ShapeDtypeStruct((layers, tq, width), BF16)]
         + [jax.ShapeDtypeStruct((tk, width), F32)] * 4,
+        input_output_aliases={7: 0} if extra else {},
         compiler_params=pltpu.CompilerParams(dimension_semantics=('arbitrary',),
                                              vmem_limit_bytes=48 * 1024 * 1024),
         cost_estimate=pl.CostEstimate(flops=flops, bytes_accessed=2 * (2 * tq * width * 2 + 4 * tk * width) + 16 * tk * width,
                                       transcendentals=tq * 2 * tk * (width // HEAD_DIM)),
         name='attn_bwd',
-    )(q, kv, kv_s, kv, kv_s, d_ctx, lse)
+    )(q, kv, kv_s, kv, kv_s, d_ctx, lse, *extra)
 
 
 GELU_C = 0.7978845608028654
@@ -276,6 +292,27 @@
     )(d_next, h, z, w1t, w2, *extra)
 
 
+def gather_pieces(part_a, part_b):
+    xa, xb = pp_x(part_a), pp_x(part_b)
+    ya, yb = pp_y(part_a), pp_y(part_b)
+    da, db = pp_y(xa), pp_x(yb)
+    own = [(xa, xb), (ya, yb), (da, db)]
+    return own, [(pp_d(a), pp_d(b)) for a, b in own]
+
+
+def reduce_pieces(piece):
+    total = {}
+    for r in (3, 1, 2, 0):
+        for part in (0, 1):
+            total[r, part] = piece(r, 0, part) + pp_d(piece(r, 1, part))
+    a0 = total[0, 0] + pp_x(total[1, 0])
+    a2 = total[2, 0] + pp_x(total[3, 0])
+    b0 = total[0, 1] + pp_y(total[2, 1])
+    b1 = total[1, 1] + pp_y(total[3, 1])
+    own = (a0 + pp_y(a2), b0 + pp_x(b1))
+    return own, (pp_d(own[0]), pp_d(own[1]))
+
+
 BOTH = ('model', 'data')
 
 
@@ -291,10 +328,19 @@
         chip = lax.axis_index('model')
         chip_x = lax.rem(chip, 2)
         chip_y = lax.div(chip, 2)
-
-        def take(v, which, axis, parts=2):
-            size = v.shape[axis] // parts
+        nbr_x = chip + 1 - 2 * chip_x
+        nbr_y = lax.rem(chip + 2, 4)
+        diag = lax.rem(nbr_x + 2, 4)
+        chips = (chip, nbr_x, nbr_y, diag)
+        hid = w_q.shape[1]
+        half_d = dim // 2
+        quart = half_d // 2
+
+        def take(v, which, axis, size):
             return lax.dynamic_slice_in_dim(v, which * size, size, axis)
+
+        def put(buf, v, which, axis):
+            return lax.dynamic_update_slice_in_dim(buf, v, which * v.shape[axis], axis)
 
         def gather(v):
             return lax.all_gather(v, BOTH, axis=0, tiled=True)
@@ -302,23 +348,41 @@
         def scatter(v):
             return lax.psum_scatter(v, BOTH, scatter_dimension=0, tiled=True)
 
+        def ordered(own, sib, axis):
+            size = own.shape[axis]
+            shape = own.shape[:axis] + (2 * size,) + own.shape[axis + 1:]
+            return put(put(jnp.zeros(shape, own.dtype), own, core, axis), sib, 1 - core, axis)
+
+        def keep(hist, v, layer):
+            if hist is None:
+                hist = jnp.zeros((layer_count,) + v.shape, v.dtype)
+            return lax.dynamic_update_slice(hist, v[None], (layer, 0, 0))
+
         def my_tokens(v):
             mine = lax.dynamic_index_in_dim(v, chip_x, 0, keepdims=False)
-            recv = pp_d(take(mine, 1 - core, 0))
-            return jnp.where(core == chip_y, take(mine, core, 0), recv)
-
-        wk = gather(take(w_k, core, 1).T)
-        wv = gather(take(w_v, core, 1).T)
-        wq = gather(take(w_q, core, 1).T)
-        wo = gather(take(w_o, core, 0))
-        w1 = gather(take(w_1, core, 1).T)
-        w2 = gather(take(w_2, core, 0))
+            half = mine.shape[0] // 2
+            recv = pp_d(take(mine, 1 - core, 0, half))
+            return jnp.where(core == chip_y, take(mine, core, 0, half), recv)
+
+        own_2 = take(w_2, core, 0, w_2.shape[0] // 2)
+        rows = own_2.shape[0] // 2
+        p2_own, p2_sib = gather_pieces(own_2[:rows], own_2[rows:])
+        wk = gather(take(w_k, core, 1, hid // 2).T)
+        wv = gather(take(w_v, core, 1, hid // 2).T)
+        wq = gather(take(w_q, core, 1, hid // 2).T)
+        wo = gather(take(w_o, core, 0, hid // 2))
+        w1 = gather(take(w_1, core, 1, w_1.shape[1] // 2).T)
+        w2 = put(jnp.zeros((4 * w_2.shape[0], dim), BF16), w_2, chip, 0)
+        for r in (1, 2, 3):
+            for part in (0, 1):
+                w2 = put(w2, p2_own[r - 1][part], 4 * chips[r] + 2 * core + part, 0)
+                w2 = put(w2, p2_sib[r - 1][part], 4 * chips[r] + 2 * (1 - core) + part, 0)
 
         x_cur = my_tokens(x_in)
         d_cur = my_tokens(cot_out)
 
         saved = []
-        g_hist = None
+        g_hist = u_hist = m_hist = ctx_hist = None
         for layer in range(layer_count):
             s = x_cur.astype(F32) + step_emb[layer].astype(F32)
             u = rms_norm(s).astype(BF16)
@@ -329,50 +393,67 @@
             h = (s + nn(ctx, wo)).astype(BF16)
             m = rms_norm(h.astype(F32)).astype(BF16)
             z, g_hist, x_next = mlp_fwd(m, h, w1, w2, layer, layer_count, g_hist)
-            saved.append((x_cur, u, q, kv, kv_s, ctx, lse, h, m, z))
+            u_hist, m_hist, ctx_hist = keep(u_hist, u, layer), keep(m_hist, m, layer), keep(ctx_hist, ctx, layer)
+            saved.append((x_cur, q, kv, kv_s, lse, h, z))
             x_cur = x_next
 
-        hist = []
-        up_hist = None
+        def flat(v):
+            return v.reshape(-1, v.shape[-1])
+
+        up_hist = next_hist = mid_hist = dq_hist = dkv_hist = None
         for layer in reversed(range(layer_count)):
-            x_l, u, q, kv, kv_s, ctx, lse, h, m, z = saved[layer]
+            x_l, q, kv, kv_s, lse, h, z = saved[layer]
             d_next = d_cur
+            next_hist = keep(next_hist, d_next, layer)
             if layer == 0:
-                next_h = jnp.concatenate([d_next] + [e[0] for e in reversed(hist)], axis=0)
-                term_2, d_next = lax.optimization_barrier((tn(g_hist.reshape(-1, g_hist.shape[-1]), next_h), d_next))
+                term_2, d_next = lax.optimization_barrier((tn(flat(g_hist), flat(next_hist)), d_next))
                 grad_2 = scatter(term_2)
             up_hist, d_mid = mlp_bwd(d_next, h, z, w1, w2, layer, layer_count, up_hist)
+            mid_hist = keep(mid_hist, d_mid, layer)
             if layer == 0:
-                m_h = jnp.concatenate([m] + [e[1] for e in reversed(hist)], axis=0)
-                term_1, d_mid = lax.optimization_barrier((tn(up_hist.reshape(-1, up_hist.shape[-1]), m_h), d_mid))
+                term_1, d_mid = lax.optimization_barrier((tn(flat(up_hist), flat(m_hist)), d_mid))
                 grad_1 = scatter(term_1)
-                mid_h = jnp.concatenate([d_mid] + [e[2] for e in reversed(hist)], axis=0)
-                ctx_h = jnp.concatenate([ctx] + [e[3] for e in reversed(hist)], axis=0)
-                term_o, d_mid = lax.optimization_barrier((tn(ctx_h, mid_h), d_mid))
-                grad_o = scatter(term_o)
             d_ctx = nt(d_mid, wo).astype(BF16)
-            dq, dko, dks, dvo, dvs = attn_bwd(q, kv, kv_s, d_ctx, lse)
+            dq_hist, dko, dks, dvo, dvs = attn_bwd(q, kv, kv_s, d_ctx, lse, layer, layer_count, dq_hist)
             dk = (dko + pp_d(dks)).astype(BF16)
             dv = (dvo + pp_d(dvs)).astype(BF16)
-            d_norm1 = (nn(dq, wq) + nn(dk, wk) + nn(dv, wv)).astype(BF16)
+            dkv_hist = keep(dkv_hist, jnp.concatenate([dk, dv], axis=1), layer)
+            d_norm1 = (nn(dq_hist[layer], wq) + nn(dk, wk) + nn(dv, wv)).astype(BF16)
             s = x_l.astype(F32) + step_emb[layer].astype(F32)
             norm_pull_x = jax.vjp(rms_norm, s)[1]
             d_cur = (d_mid.astype(F32) + norm_pull_x(d_norm1.astype(F32))[0]).astype(BF16)
-            hist.append((d_next, m, d_mid, ctx, u, dq, dk, dv))
-
-        u_h, dq_h, dk_h, dv_h = [jnp.concatenate([e[i] for e in reversed(hist)], axis=0) for i in (4, 5, 6, 7)]
-        grad_q = scatter(tn(dq_h, u_h))
-        grad_k = scatter(tn(dk_h, u_h))
-        grad_v = scatter(tn(dv_h, u_h))
-        d_x = lax.dynamic_slice_in_dim(gather(d_cur).reshape((4, 1024, dim)), 2 * core, 2, 0)
-
-        def whole(v):
-            other = pp_d(v)
-            size = v.shape[0]
-            out = lax.dynamic_update_slice_in_dim(jnp.zeros((2 * size,) + v.shape[1:], v.dtype), v, core * size, 0)
-            return lax.dynamic_update_slice_in_dim(out, other, (1 - core) * size, 0)
-
-        return (whole(grad_q).T, whole(grad_k).T, whole(grad_v).T, whole(grad_o), whole(grad_1).T, whole(grad_2), d_x)
+
+        def fixed(v):
+            return lax.optimization_barrier(v)
+
+        ctx_f, dq_f, dkv_f, mid_f, u_f = flat(ctx_hist), flat(dq_hist), flat(dkv_hist), flat(mid_hist), flat(u_hist)
+        mid_half = [fixed(take(mid_f, w, 1, half_d)) for w in (core, 1 - core)]
+        u_half = [fixed(take(u_f, w, 1, half_d)) for w in (core, 1 - core)]
+        ctx_r = [fixed(take(ctx_f, c, 1, hid)) for c in chips]
+        dqkv_r = [fixed(jnp.concatenate([take(dq_f, c, 1, hid), take(dkv_f, c, 1, hid), take(dkv_f, 4 + c, 1, hid)], axis=1))
+                  for c in chips]
+
+        def piece_o(r, half, part):
+            return tn(ctx_r[r], mid_half[half][:, part * quart:(part + 1) * quart])
+
+        def piece_qkv(r, half, part):
+            return tn(u_half[half][:, part * quart:(part + 1) * quart], dqkv_r[r])
+
+        own, sib = reduce_pieces(piece_o)
+        grad_o = ordered(jnp.concatenate(own, 1), jnp.concatenate(sib, 1), 1)
+        own, sib = reduce_pieces(piece_qkv)
+        grad_qkv = ordered(jnp.concatenate(own, 0), jnp.concatenate(sib, 0), 0)
+
+        whole = ordered(d_cur, pp_d(d_cur), 0)
+        to_row = [(2 * c + d, 2 * (c ^ 2) + d) for c in range(4) for d in range(2) if c // 2 == d]
+        from_y = lax.ppermute(whole, BOTH, to_row)
+        row_seq = jnp.where(chip_y == core, whole, from_y)
+        d_x = jnp.zeros((2,) + whole.shape, BF16)
+        d_x = put(put(d_x, row_seq[None], chip_x, 0), pp_x(row_seq)[None], 1 - chip_x, 0)
+
+        grad_1 = ordered(grad_1, pp_d(grad_1), 0).T
+        grad_2 = ordered(grad_2, pp_d(grad_2), 0)
+        return (grad_qkv[:, :hid], grad_qkv[:, hid:2 * hid], grad_qkv[:, 2 * hid:], grad_o, grad_1, grad_2, d_x)
 
     return jax.shard_map(device_step, mesh=mesh,
                          in_specs=(spec_act, spec_act, spec_rep, spec_col, spec_col, spec_col, spec_row, spec_col, spec_row),

time: 1880 us -> 1710 us (0.910)
  waiting for transfers between devices: 914 us -> 574 us
  local copies, waits for them, and re-layouts: 86.7 us -> 167 us
  starting transfers between devices: 5.6 us -> 37.8 us
  other arithmetic: 28.2 us -> 59.8 us
  matrix products: 301 us -> 328 us
    reduce_scatter x6 -> x2, waiting for transfers between devices: 555 us -> 0.01 us  [scatter(): return lax.psum_scatter(v, BOTH, scatter_dimension=0, tiled=True)]
    ppermute x0 -> x20, waiting for transfers between devices: none -> 464 us  [the longest x10 241 us: pp_x(): return lax.ppermute(v, 'model', SWAP_X)]
    all_gather x7 -> x5, waiting for transfers between devices: 315 us -> 85.2 us  [gather(): return lax.all_gather(v, BOTH, axis=0, tiled=True)]
    dynamic_update_slice x12 -> x31, local copies, waits for them, and re-layouts: 24.2 us -> 67.9 us  [the longest x21 48 us: put(): return lax.dynamic_update_slice_in_dim(buf, v, which * v.shape[axis], axis)]
    dynamic_update_slice x0 -> x15, other arithmetic: none -> 31.3 us  [the longest x11 20.1 us: keep(): return lax.dynamic_update_slice(hist, v[None], (layer, 0, 0))]
    ppermute x0 -> x20, starting transfers between devices: none -> 28.2 us  [the longest x10 14.1 us: pp_x(): return lax.ppermute(v, 'model', SWAP_X)]
    dot_general x38 -> x66, matrix products: 301 us -> 328 us  [dot(): return lax.dot_general(a, b, (dims, ((), ())), preferred_element_type=F32)]
    ppermute x20 -> x43, waiting for transfers between devices: 42.4 us -> 24.5 us  [pp_d(): return lax.ppermute(v, 'data', SWAP_D)]
  transfers between devices with their start and end apart: 33 -> 70, of which waited for: 22 -> 21; matrix products, arithmetic and copies ran while one was open for 12% -> 20% of each run, Pallas kernels for 4% -> 4%
where the time goes in v3:
time: 1710 us; the launch traced here: 1700 us
  waiting for transfers between devices  574 us (34%)
  Pallas kernels  521 us (30%)
  matrix products  328 us (19%)
  local copies, waits for them, and re-layouts  167 us (10%)
  other arithmetic  59.8 us (3%)
  starting transfers between devices  37.8 us (2%)
    dot_general x66, matrix products, dot(): return lax.dot_general(a, b, (dims, ((), ())), preferred_element_type=F32)  328 us
    ppermute x10, waiting for transfers between devices, pp_x(): return lax.ppermute(v, 'model', SWAP_X)  241 us
    ppermute x9, waiting for transfers between devices, pp_y(): return lax.ppermute(v, 'model', SWAP_Y)  223 us
    pallas_call x4, Pallas kernels, attn_bwd(): pl.pallas_call(attn_bwd_body, grid=(pairs,), in_specs=[pl.BlockSpec((tq,...  197 us
    pallas_call x4, Pallas kernels, mlp_bwd(): pl.pallas_call(mlp_bwd_body, grid=(hidden // BLOCK_F,), in_specs=[whole,...  119 us
    pallas_call x4, Pallas kernels, mlp_fwd(): pl.pallas_call(mlp_fwd_body, grid=(hidden // BLOCK_F,), in_specs=[whole,...  110 us
    pallas_call x4, Pallas kernels, attn_fwd(): pl.pallas_call(attn_fwd_body, grid=(pairs,), in_specs=[pl.BlockSpec((tq,...  95.7 us
    all_gather x5, waiting for transfers between devices, gather(): return lax.all_gather(v, BOTH, axis=0, tiled=True)  85.2 us
  transfers between devices with their start and end apart: 70, of which 21 were waited for; matrix products, arithmetic and copies ran while one was open for 20% of the time, Pallas kernels for 4%

profile of v3, /device:TPU:0, one launch (start us, length us, event | category | flops | bytes accessed | tf_op | source)
XLA Modules:
  0.0 1703.8 jit_solution(14160312074158980727)
XLA Ops:
  29.8 35.4 %collective-permute-done.2 = bf16[384,1536]{1,0:T(8,128)(2,1)} collective-permute-done((bf16[384,1536]{1,0:T(8,128)(2,1)}, bf16[384,1536]{1,0:T(8,128)(2,1)}, u32[]{:S(2)}, u32[]{:S(2)}) %collective-permute-start.2) | collective-permute-done | bytes 1179680 | tf_op jit(solution)/shard_map/ppermute | solution.py:24
  65.2 6.8 broadcast_in_dim.128
  82.1 23.7 %collective-permute-done.4 = bf16[384,1536]{1,0:T(8,128)(2,1)} collective-permute-done((bf16[384,1536]{1,0:T(8,128)(2,1)}, bf16[384,1536]{1,0:T(8,128)(2,1)}, u32[]{:S(2)}, u32[]{:S(2)}) %collective-permute-start.4) | collective-permute-done | bytes 1179680 | tf_op jit(solution)/shard_map/ppermute | solution.py:24
  107.2 6.5 collective-permute-done.6
  116.7 5.0 convolution_convert_fusion.13
  121.8 5.2 convolution_convert_fusion.14
  131.5 16.3 collective-permute-done.10
  167.4 5.0 convolution_convert_fusion.15.q_ref.refs_0_
  172.4 23.7 %attn_fwd.4 = (bf16[512,1536]{1,0:T(8,128)(2,1)S(1)}, f32[12,2,512]{2,1,0:T(2,128)S(1)}) custom-call(bf16[512,1536]{1,0:T(8,128)(2,1)S(1)} %convolution_convert_fusion.15.q_ref.refs_0_, bf16[512,3072]{1,0:T(8,128)(2,1)} %pad_maximum_fusion.4.ko_ref.vo_ref.refs_1_.refs_3_, bf16[512,3072]{1,0:T(8,128)(2,1)} %collective-permute-done.1.ks_ref.vs_ref.refs_2_.refs_4_, ...), custom_call_target="tpu_custom_call" | custom-call | flops 12884901888 | bytes 9437184 | tf_op jit(solution)/shard_map/attn_fwd/pallas_call | solution.py:95
  197.3 6.6 fusion
  204.3 85.2 %all-gather.14.cloned.1.call-done.refs_2_.refs_3_ = bf16[6144,1536]{1,0:T(8,128)(2,1)} async-done(((bf16[768,1536]{1,0:T(8,128)(2,1)}), bf16[6144,1536]{1,0:T(8,128)(2,1)}) %all-gather.14.cloned.1.call-update) | async-done | bytes 18874384 | tf_op jit(solution)/shard_map/all_gather | solution.py:346
  289.5 27.0 %mlp_fwd.4 = (bf16[512,6144]{1,0:T(8,128)(2,1)}, bf16[4,512,6144]{2,1,0:T(8,128)(2,1)}, bf16[512,1536]{1,0:T(8,128)(2,1)S(1)}) custom-call(bf16[512,1536]{1,0:T(8,128)(2,1)S(1)} %fusion.1.refs_0_, bf16[512,1536]{1,0:T(8,128)(2,1)S(1)} %get-tuple-element.174.refs_1_, bf16[6144,1536]{1,0:T(8,128)(2,1)} %all-gather.14.cloned.1.call-done.refs_2_.refs_3_, ...), custom_call_target="tpu_custom_call" | custom-call | flops 19327352832 | bytes 50331648 | tf_op jit(solution)/shard_map/mlp_fwd/pallas_call | solution.py:225
  317.7 5.0 convolution_convert_fusion.11
  322.6 5.0 convolution_convert_fusion.10
  336.5 24.2 %attn_fwd.5 = (bf16[512,1536]{1,0:T(8,128)(2,1)S(1)}, f32[12,2,512]{2,1,0:T(2,128)S(1)}) custom-call(bf16[512,1536]{1,0:T(8,128)(2,1)S(1)} %convolution_convert_fusion.12.q_ref.refs_0_, bf16[512,3072]{1,0:T(8,128)(2,1)} %copy-done.58, bf16[512,3072]{1,0:T(8,128)(2,1)} %collective-permute-done.14.ks_ref.vs_ref.refs_2_.refs_4_, bf16[512,3072]{1,0:T(8,128)(2,1)} %copy-done.58, ...), custom_call_target="tpu_custom_call" | custom-call | flops 12884901888 | bytes 9437184 | tf_op jit(solution)/shard_map/attn_fwd/pallas_call | solution.py:95
  360.7 5.6 fusion.2
  367.9 28.0 %mlp_fwd.5 = (bf16[512,6144]{1,0:T(8,128)(2,1)}, bf16[4,512,6144]{2,1,0:T(8,128)(2,1)}, bf16[512,1536]{1,0:T(8,128)(2,1)S(1)}) custom-call(bf16[512,1536]{1,0:T(8,128)(2,1)S(1)} %get-tuple-element.136.refs_0_, bf16[512,1536]{1,0:T(8,128)(2,1)S(1)} %get-tuple-element.176.refs_1_, ...), custom_call_target="tpu_custom_call", output_to_operand_aliasing={{1}: (4, {})} | custom-call | flops 19327352832 | bytes 50331648 | tf_op jit(solution)/shard_map/mlp_fwd/pallas_call | solution.py:225
  399.1 5.0 convolution_convert_fusion.7
  412.0 23.7 %attn_fwd.6 = (bf16[512,1536]{1,0:T(8,128)(2,1)S(1)}, f32[12,2,512]{2,1,0:T(2,128)S(1)}) custom-call(bf16[512,1536]{1,0:T(8,128)(2,1)S(1)} %convolution_convert_fusion.9.q_ref.refs_0_, bf16[512,3072]{1,0:T(8,128)(2,1)} %copy-done.59, bf16[512,3072]{1,0:T(8,128)(2,1)} %copy-done.103, bf16[512,3072]{1,0:T(8,128)(2,1)} %copy-done.59, bf16[512,3072]{1,0:T(8,128)(2,1)} %copy-done.103), custom_call_target="tpu_custom_call" | custom-call | flops 12884901888 | bytes 9437184 | tf_op jit(solution)/shard_map/attn_fwd/pallas_call | solution.py:95
  435.7 5.7 fusion.4
  443.1 27.3 %mlp_fwd.6 = (bf16[512,6144]{1,0:T(8,128)(2,1)}, bf16[4,512,6144]{2,1,0:T(8,128)(2,1)}, bf16[512,1536]{1,0:T(8,128)(2,1)S(1)}) custom-call(bf16[512,1536]{1,0:T(8,128)(2,1)S(1)} %get-tuple-element.134.refs_0_, bf16[512,1536]{1,0:T(8,128)(2,1)S(1)} %get-tuple-element.178.refs_1_, ...), custom_call_target="tpu_custom_call", output_to_operand_aliasing={{1}: (4, {})} | custom-call | flops 19327352832 | bytes 50331648 | tf_op jit(solution)/shard_map/mlp_fwd/pallas_call | solution.py:225
  473.5 5.1 convolution_convert_fusion.4
  480.1 7.0 collective-permute-done.17
  490.4 24.1 %attn_fwd.7 = (bf16[512,1536]{1,0:T(8,128)(2,1)S(1)}, f32[12,2,512]{2,1,0:T(2,128)S(1)}) custom-call(bf16[512,1536]{1,0:T(8,128)(2,1)S(1)} %convolution_convert_fusion.6.q_ref.refs_0_, bf16[512,3072]{1,0:T(8,128)(2,1)} %copy-done.60, bf16[512,3072]{1,0:T(8,128)(2,1)} %collective-permute-done.16.ks_ref.vs_ref.refs_2_.refs_4_, bf16[512,3072]{1,0:T(8,128)(2,1)} %copy-done.60, ...), custom_call_target="tpu_custom_call" | custom-call | flops 12884901888 | bytes 9437184 | tf_op jit(solution)/shard_map/attn_fwd/pallas_call | solution.py:95
  514.5 5.6 fusion.6
  521.6 27.5 %mlp_fwd.7 = (bf16[512,6144]{1,0:T(8,128)(2,1)}, bf16[4,512,6144]{2,1,0:T(8,128)(2,1)}, bf16[512,1536]{1,0:T(8,128)(2,1)}) custom-call(bf16[512,1536]{1,0:T(8,128)(2,1)S(1)} %get-tuple-element.132.refs_0_, bf16[512,1536]{1,0:T(8,128)(2,1)S(1)} %get-tuple-element.180.refs_1_, ...), custom_call_target="tpu_custom_call", output_to_operand_aliasing={{1}: (4, {})} | custom-call | flops 19327352832 | bytes 50331648 | tf_op jit(solution)/shard_map/mlp_fwd/pallas_call | solution.py:225
  549.1 29.7 %mlp_bwd.4 = (bf16[4,512,6144]{2,1,0:T(8,128)(2,1)}, bf16[512,1536]{1,0:T(8,128)(2,1)S(1)}) custom-call(bf16[512,1536]{1,0:T(8,128)(2,1)S(1)} %bitcast_select_fusion.refs_0_, bf16[512,1536]{1,0:T(8,128)(2,1)S(1)} %get-tuple-element.180.refs_1_, bf16[512,6144]{1,0:T(8,128)(2,1)} %get-tuple-element.69.refs_2_, ...), custom_call_target="tpu_custom_call" | custom-call | flops 19327352832 | bytes 50331648 | tf_op jit(solution)/shard_map/mlp_bwd/pallas_call | solution.py:279
  578.9 5.0 convolution_convert_fusion.3.refs_5_
  583.9 49.2 %attn_bwd.4 = (bf16[4,512,1536]{2,1,0:T(8,128)(2,1)}, f32[512,1536]{1,0:T(8,128)}, f32[512,1536]{1,0:T(8,128)}, f32[512,1536]{1,0:T(8,128)}, f32[512,1536]{1,0:T(8,128)}) custom-call(bf16[512,1536]{1,0:T(8,128)(2,1)S(1)} %convolution_convert_fusion.6.q_ref.refs_0_, bf16[512,3072]{1,0:T(8,128)(2,1)} %copy-done.60, ...), custom_call_target="tpu_custom_call" | custom-call | flops 32212254720 | bytes 25165824 | tf_op jit(solution)/shard_map/attn_bwd/pallas_call | solution.py:164
  645.2 5.3 convolution_add_fusion.7
  659.3 29.6 %mlp_bwd.5 = (bf16[4,512,6144]{2,1,0:T(8,128)(2,1)}, bf16[512,1536]{1,0:T(8,128)(2,1)S(1)}) custom-call(bf16[512,1536]{1,0:T(8,128)(2,1)S(1)} %get-tuple-element.142.refs_0_, bf16[512,1536]{1,0:T(8,128)(2,1)S(1)} %copy-done.9, bf16[512,6144]{1,0:T(8,128)(2,1)} %get-tuple-element.77.refs_2_, ...), custom_call_target="tpu_custom_call", output_to_operand_aliasing={{0}: (5, {})} | custom-call | flops 19327352832 | bytes 50331648 | tf_op jit(solution)/shard_map/mlp_bwd/pallas_call | solution.py:279
  688.9 5.1 convolution_convert_fusion.2.refs_5_
  694.0 49.3 %attn_bwd.5 = (bf16[4,512,1536]{2,1,0:T(8,128)(2,1)}, f32[512,1536]{1,0:T(8,128)}, f32[512,1536]{1,0:T(8,128)}, f32[512,1536]{1,0:T(8,128)}, f32[512,1536]{1,0:T(8,128)}) custom-call(bf16[512,1536]{1,0:T(8,128)(2,1)S(1)} %copy-done.23, bf16[512,3072]{1,0:T(8,128)(2,1)} %copy-done.59, bf16[512,3072]{1,0:T(8,128)(2,1)} %copy-done.103, ...), custom_call_target="tpu_custom_call", output_to_operand_aliasing={{0}: (7, {})} | custom-call | flops 32212254720 | bytes 25165824 | tf_op jit(solution)/shard_map/attn_bwd/pallas_call | solution.py:164
  750.0 5.1 fusion.113
  768.0 29.9 %mlp_bwd.6 = (bf16[4,512,6144]{2,1,0:T(8,128)(2,1)}, bf16[512,1536]{1,0:T(8,128)(2,1)S(1)}) custom-call(bf16[512,1536]{1,0:T(8,128)(2,1)S(1)} %get-tuple-element.140.refs_0_, bf16[512,1536]{1,0:T(8,128)(2,1)S(1)} %copy-done.7, bf16[512,6144]{1,0:T(8,128)(2,1)} %get-tuple-element.86.refs_2_, ...), custom_call_target="tpu_custom_call", output_to_operand_aliasing={{0}: (5, {})} | custom-call | flops 19327352832 | bytes 50331648 | tf_op jit(solution)/shard_map/mlp_bwd/pallas_call | solution.py:279
  800.6 48.8 %attn_bwd.6 = (bf16[4,512,1536]{2,1,0:T(8,128)(2,1)}, f32[512,1536]{1,0:T(8,128)}, f32[512,1536]{1,0:T(8,128)}, f32[512,1536]{1,0:T(8,128)}, f32[512,1536]{1,0:T(8,128)}) custom-call(bf16[512,1536]{1,0:T(8,128)(2,1)S(1)} %copy-done.21, bf16[512,3072]{1,0:T(8,128)(2,1)} %copy-done.58, ...), custom_call_target="tpu_custom_call", output_to_operand_aliasing={{0}: (7, {})} | custom-call | flops 32212254720 | bytes 25165824 | tf_op jit(solution)/shard_map/attn_bwd/pallas_call | solution.py:164
  849.9 5.4 collective-permute-done.22
  857.8 5.1 fusion.114
  874.2 45.5 %convolution_bitcast_fusion.1 = f32[6144,1536]{1,0:T(8,128)} fusion(bf16[4,512,6144]{2,1,0:T(8,128)(2,1)} %get-tuple-element.68, bf16[4,512,1536]{2,1,0:T(8,128)(2,1)S(1)} %get-tuple-element.137), kind=kOutput, calls=%fused_computation.1 | convolution fusion | flops 38654705664 | bytes 69206016 | tf_op jit(solution)/shard_map/dot_general | solution.py:40
  921.2 29.6 %mlp_bwd.7 = (bf16[4,512,6144]{2,1,0:T(8,128)(2,1)}, bf16[512,1536]{1,0:T(8,128)(2,1)S(1)}) custom-call(bf16[512,1536]{1,0:T(8,128)(2,1)S(1)} %copy-done.5, bf16[512,1536]{1,0:T(8,128)(2,1)S(1)} %get-tuple-element.174.refs_1_, bf16[512,6144]{1,0:T(8,128)(2,1)} %get-tuple-element.96.refs_2_, ...), custom_call_target="tpu_custom_call", output_to_operand_aliasing={{0}: (5, {})} | custom-call | flops 19327352832 | bytes 50331648 | tf_op jit(solution)/shard_map/mlp_bwd/pallas_call | solution.py:279
  950.8 47.7 %convolution_bitcast_fusion = f32[6144,1536]{1,0:T(8,128)} fusion(bf16[4,512,6144]{2,1,0:T(8,128)(2,1)} %get-tuple-element.98, bf16[4,512,1536]{2,1,0:T(8,128)(2,1)} %get-tuple-element.131), kind=kOutput, calls=%fused_computation | convolution fusion | flops 38654705664 | bytes 69206016 | tf_op jit(solution)/shard_map/dot_general | solution.py:40
  1009.2 11.3 dynamic_update_slice.172
  1024.4 6.1 convolution_convert_fusion.refs_5_
  1030.5 49.2 %attn_bwd.7 = (bf16[4,512,1536]{2,1,0:T(8,128)(2,1)}, f32[512,1536]{1,0:T(8,128)}, f32[512,1536]{1,0:T(8,128)}, f32[512,1536]{1,0:T(8,128)}, f32[512,1536]{1,0:T(8,128)}) custom-call(bf16[512,1536]{1,0:T(8,128)(2,1)S(1)} %copy-done.19, bf16[512,3072]{1,0:T(8,128)(2,1)} %pad_maximum_fusion.4.ko_ref.vo_ref.refs_1_.refs_3_, ...), custom_call_target="tpu_custom_call", output_to_operand_aliasing={{0}: (7, {})} | custom-call | flops 32212254720 | bytes 25165824 | tf_op jit(solution)/shard_map/attn_bwd/pallas_call | solution.py:164
  1080.2 5.8 constant_dynamic-slice_fusion.5
  1088.4 5.6 constant_dynamic-slice_fusion.6
  1116.5 23.1 %collective-permute-done.47 = f32[384,384]{0,1:T(8,128)S(1)} collective-permute-done((f32[384,384]{0,1:T(8,128)S(1)}, f32[384,384]{0,1:T(8,128)S(1)}, u32[]{:S(2)}, u32[]{:S(2)}) %collective-permute-start.47) | collective-permute-done | bytes 589856 | tf_op jit(solution)/shard_map/ppermute | solution.py:24
  1145.7 21.6 %collective-permute-done.54 = f32[384,384]{0,1:T(8,128)S(1)} collective-permute-done((f32[384,384]{0,1:T(8,128)S(1)}, f32[384,384]{0,1:T(8,128)S(1)}, u32[]{:S(2)}, u32[]{:S(2)}) %collective-permute-start.54) | collective-permute-done | bytes 589856 | tf_op jit(solution)/shard_map/ppermute | solution.py:28
  1173.0 15.2 collective-permute-done.48
  1192.5 7.1 fusion.115
  1202.3 8.5 convolution_add_fusion.1
  1210.8 5.3 fusion.11
  1286.9 40.9 %collective-permute-done.31 = f32[384,1152]{1,0:T(8,128)} collective-permute-done((f32[384,1152]{1,0:T(8,128)S(1)}, f32[384,1152]{1,0:T(8,128)}, u32[]{:S(2)}, u32[]{:S(2)}) %collective-permute-start.31) | collective-permute-done | bytes 1769504 | tf_op jit(solution)/shard_map/ppermute | solution.py:24
  1327.8 5.5 fusion.26
  1333.3 115.8 %collective-permute-done.51 = f32[384,384]{0,1:T(8,128)S(1)} collective-permute-done((f32[384,384]{0,1:T(8,128)S(1)}, f32[384,384]{0,1:T(8,128)S(1)}, u32[]{:S(2)}, u32[]{:S(2)}) %collective-permute-start.51) | collective-permute-done | bytes 589856 | tf_op jit(solution)/shard_map/ppermute | solution.py:28
  1457.1 10.5 collective-permute-done.55
  1475.4 58.4 %collective-permute-done.28 = f32[384,1152]{1,0:T(8,128)} collective-permute-done((f32[384,1152]{1,0:T(8,128)}, f32[384,1152]{1,0:T(8,128)}, u32[]{:S(2)}, u32[]{:S(2)}) %collective-permute-start.28) | collective-permute-done | bytes 1769504 | tf_op jit(solution)/shard_map/ppermute | solution.py:24
  1534.3 5.7 fusion.28
  1542.7 47.4 %collective-permute-done.35 = f32[384,1152]{1,0:T(8,128)} collective-permute-done((f32[384,1152]{1,0:T(8,128)}, f32[384,1152]{1,0:T(8,128)}, u32[]{:S(2)}, u32[]{:S(2)}) %collective-permute-start.35) | collective-permute-done | bytes 1769504 | tf_op jit(solution)/shard_map/ppermute | solution.py:28
  1594.3 7.8 fusion.25
  1617.7 43.9 %collective-permute-done.62 = bf16[1024,1536]{1,0:T(8,128)(2,1)} collective-permute-done((bf16[1024,1536]{1,0:T(8,128)(2,1)}, bf16[1024,1536]{1,0:T(8,128)(2,1)}, u32[]{:S(2)}, u32[]{:S(2)}) %collective-permute-start.62) | collective-permute-done | bytes 3145760 | tf_op jit(solution)/shard_map/ppermute | solution.py:24
  1667.3 5.1 broadcast.163.clone
  1677.3 4.9 constant_dynamic-update-slice_fusion.4
  1682.2 9.7 copy.67
  (614 shorter events, 337.1 us)
Async XLA Ops:
  7.2 109.5 %all-gather.10.cloned.1.call-start = ((), (), s32[]{:S(2)}) async-start(), calls=%async_computation.4 | async-start | bytes 5308416 | tf_op jit(solution)/shard_map/all_gather | solution.py:346
  9.9 111.9 %all-gather.8.cloned.1.call-start = ((), (), s32[]{:S(2)}) async-start(), calls=%async_computation.3 | async-start | bytes 5308416 | tf_op jit(solution)/shard_map/all_gather | solution.py:346
  11.4 156.0 %all-gather.6.cloned.1.call-start = ((), (), s32[]{:S(2)}) async-start(), calls=%async_computation.2 | async-start | bytes 5308416 | tf_op jit(solution)/shard_map/all_gather | solution.py:346
  12.9 184.5 %all-gather.12.cloned.1.call-start = ((), (), s32[]{:S(2)}) async-start(), calls=%async_computation.5 | async-start | bytes 5308416 | tf_op jit(solution)/shard_map/all_gather | solution.py:346
  13.8 275.7 %all-gather.14.cloned.1.call-start = ((), (), s32[]{:S(2)}) async-start(), calls=%async_computation.6 | async-start | bytes 21233664 | tf_op jit(solution)/shard_map/all_gather | solution.py:346
  18.2 1576.0 %reduce-scatter.3.cloned.1.call-start = ((), (), s32[]{:S(2)}) async-start(), calls=%async_computation.7 | async-start | bytes 42467328 | tf_op jit(solution)/shard_map/reduce_scatter | solution.py:349
  21.6 43.7 %collective-permute-start.2 = (bf16[384,1536]{1,0:T(8,128)(2,1)}, bf16[384,1536]{1,0:T(8,128)(2,1)}, u32[]{:S(2)}, u32[]{:S(2)}) collective-permute-start(bf16[384,1536]{1,0:T(8,128)(2,1)} %get-tuple-element.169), channel_id=1, source_target_pairs={{0,2},{2,0},{4,6},{6,4},{1,3},{3,1},{5,7},{7,5}} | collective-permute-start | bytes 3538952 | tf_op jit(solution)/shard_map/ppermute | solution.py:24
  27.7 51.3 %collective-permute-start = (bf16[512,1536]{1,0:T(8,128)(2,1)}, bf16[512,1536]{1,0:T(8,128)(2,1)S(1)}, u32[]{:S(2)}, u32[]{:S(2)}) collective-permute-start(bf16[512,1536]{1,0:T(8,128)(2,1)} %dynamic-slice_bitcast_fusion.1), channel_id=1, source_target_pairs={{0,1},{1,0},{2,3},{3,2},{4,5},{5,4},{6,7},{7,6}} | collective-permute-start | bytes 4718600 | tf_op jit(solution)/shard_map/ppermute | solution.py:32
  27.7 49.8 %collective-permute-start.8 = (bf16[384,1536]{1,0:T(8,128)(2,1)}, bf16[384,1536]{1,0:T(8,128)(2,1)}, u32[]{:S(2)}, u32[]{:S(2)}) collective-permute-start(bf16[384,1536]{1,0:T(8,128)(2,1)} %get-tuple-element.168), channel_id=1, source_target_pairs={{0,4},{4,0},{2,6},{6,2},{1,5},{5,1},{3,7},{7,3}} | collective-permute-start | bytes 3538952 | tf_op jit(solution)/shard_map/ppermute | solution.py:28
  29.3 76.5 %collective-permute-start.4 = (bf16[384,1536]{1,0:T(8,128)(2,1)}, bf16[384,1536]{1,0:T(8,128)(2,1)}, u32[]{:S(2)}, u32[]{:S(2)}) collective-permute-start(bf16[384,1536]{1,0:T(8,128)(2,1)} %get-tuple-element.168), channel_id=1, source_target_pairs={{0,2},{2,0},{4,6},{6,4},{1,3},{3,1},{5,7},{7,5}} | collective-permute-start | bytes 3538952 | tf_op jit(solution)/shard_map/ppermute | solution.py:24
  29.8 84.0 %collective-permute-start.6 = (bf16[384,1536]{1,0:T(8,128)(2,1)}, bf16[384,1536]{1,0:T(8,128)(2,1)}, u32[]{:S(2)}, u32[]{:S(2)}) collective-permute-start(bf16[384,1536]{1,0:T(8,128)(2,1)} %get-tuple-element.169), channel_id=1, source_target_pairs={{0,4},{4,0},{2,6},{6,2},{1,5},{5,1},{3,7},{7,3}} | collective-permute-start | bytes 3538952 | tf_op jit(solution)/shard_map/ppermute | solution.py:28
  65.2 48.6 %collective-permute-start.3 = (bf16[384,1536]{1,0:T(8,128)(2,1)}, bf16[384,1536]{1,0:T(8,128)(2,1)}, u32[]{:S(2)}, u32[]{:S(2)}) collective-permute-start(bf16[384,1536]{1,0:T(8,128)(2,1)} %collective-permute-done.2), channel_id=1, source_target_pairs={{0,1},{1,0},{2,3},{3,2},{4,5},{5,4},{6,7},{7,6}} | collective-permute-start | bytes 3538952 | tf_op jit(solution)/shard_map/ppermute | solution.py:32
  77.5 70.3 %collective-permute-start.10 = (bf16[384,1536]{1,0:T(8,128)(2,1)}, bf16[384,1536]{1,0:T(8,128)(2,1)}, u32[]{:S(2)}, u32[]{:S(2)}) collective-permute-start(bf16[384,1536]{1,0:T(8,128)(2,1)} %collective-permute-done.2), channel_id=1, source_target_pairs={{0,4},{4,0},{2,6},{6,2},{1,5},{5,1},{3,7},{7,3}} | collective-permute-start | bytes 3538952 | tf_op jit(solution)/shard_map/ppermute | solution.py:28
  79.0 78.8 %collective-permute-start.9 = (bf16[384,1536]{1,0:T(8,128)(2,1)}, bf16[384,1536]{1,0:T(8,128)(2,1)}, u32[]{:S(2)}, u32[]{:S(2)}) collective-permute-start(bf16[384,1536]{1,0:T(8,128)(2,1)} %collective-permute-done.8), channel_id=1, source_target_pairs={{0,1},{1,0},{2,3},{3,2},{4,5},{5,4},{6,7},{7,6}} | collective-permute-start | bytes 3538952 | tf_op jit(solution)/shard_map/ppermute | solution.py:32
  105.8 42.0 %collective-permute-start.12 = (bf16[384,1536]{1,0:T(8,128)(2,1)}, bf16[384,1536]{1,0:T(8,128)(2,1)}, u32[]{:S(2)}, u32[]{:S(2)}) collective-permute-start(bf16[384,1536]{1,0:T(8,128)(2,1)} %collective-permute-done.8), channel_id=1, source_target_pairs={{0,2},{2,0},{4,6},{6,4},{1,3},{3,1},{5,7},{7,5}} | collective-permute-start | bytes 3538952 | tf_op jit(solution)/shard_map/ppermute | solution.py:24
  113.8 15.3 collective-permute-start.5
  113.8 39.3 %collective-permute-start.7 = (bf16[384,1536]{1,0:T(8,128)(2,1)}, bf16[384,1536]{1,0:T(8,128)(2,1)}, u32[]{:S(2)}, u32[]{:S(2)}) collective-permute-start(bf16[384,1536]{1,0:T(8,128)(2,1)} %collective-permute-done.6), channel_id=1, source_target_pairs={{0,1},{1,0},{2,3},{3,2},{4,5},{5,4},{6,7},{7,6}} | collective-permute-start | bytes 3538952 | tf_op jit(solution)/shard_map/ppermute | solution.py:32
  129.1 43.4 %collective-permute-start.1 = (bf16[512,3072]{1,0:T(8,128)(2,1)}, bf16[512,3072]{1,0:T(8,128)(2,1)}, u32[]{:S(2)}, u32[]{:S(2)}) collective-permute-start(bf16[512,3072]{1,0:T(8,128)(2,1)} %pad_maximum_fusion.4.ko_ref.vo_ref.refs_1_.refs_3_), channel_id=1, source_target_pairs={{0,1},{1,0},{2,3},{3,2},{4,5},{5,4},{6,7},{7,6}} | collective-permute-start | bytes 9437192 | tf_op jit(solution)/shard_map/ppermute | solution.py:32
  147.8 14.9 collective-permute-start.11
  147.8 18.5 %collective-permute-start.13 = (bf16[384,1536]{1,0:T(8,128)(2,1)}, bf16[384,1536]{1,0:T(8,128)(2,1)S(1)}, u32[]{:S(2)}, u32[]{:S(2)}) collective-permute-start(bf16[384,1536]{1,0:T(8,128)(2,1)} %collective-permute-done.12), channel_id=1, source_target_pairs={{0,1},{1,0},{2,3},{3,2},{4,5},{5,4},{6,7},{7,6}} | collective-permute-start | bytes 3538952 | tf_op jit(solution)/shard_map/ppermute | solution.py:32
  479.2 11.2 collective-permute-start.16
  633.1 8.4 collective-permute-start.18
  637.3 13.2 collective-permute-start.19
  743.6 15.7 collective-permute-start.21
  849.7 17.4 %collective-permute-start.23 = (f32[512,1536]{1,0:T(8,128)}, f32[512,1536]{1,0:T(8,128)S(1)}, u32[]{:S(2)}, u32[]{:S(2)}) collective-permute-start(f32[512,1536]{1,0:T(8,128)} %get-tuple-element.94), channel_id=1, source_target_pairs={{0,1},{1,0},{2,3},{3,2},{4,5},{5,4},{6,7},{7,6}} | collective-permute-start | bytes 9437192 | tf_op jit(solution)/shard_map/ppermute | solution.py:32
  998.5 604.0 %reduce-scatter.5.cloned.1.call-start = ((), (), s32[]{:S(2)}) async-start(), calls=%async_computation.8 | async-start | bytes 42467328 | tf_op jit(solution)/shard_map/reduce_scatter | solution.py:349
  1079.7 110.4 %collective-permute-start.24 = (f32[512,1536]{1,0:T(8,128)}, f32[512,1536]{1,0:T(8,128)}, u32[]{:S(2)}, u32[]{:S(2)}) collective-permute-start(f32[512,1536]{1,0:T(8,128)} %get-tuple-element.104), channel_id=1, source_target_pairs={{0,1},{1,0},{2,3},{3,2},{4,5},{5,4},{6,7},{7,6}} | collective-permute-start | bytes 9437192 | tf_op jit(solution)/shard_map/ppermute | solution.py:32
  1095.9 12.2 collective-permute-start.46
  1106.9 8.9 collective-permute-start.43
  1107.0 9.4 collective-permute-start.45
  1111.0 28.6 %collective-permute-start.47 = (f32[384,384]{0,1:T(8,128)S(1)}, f32[384,384]{0,1:T(8,128)S(1)}, u32[]{:S(2)}, u32[]{:S(2)}) collective-permute-start(f32[384,384]{0,1:T(8,128)S(1)} %convolution_add_fusion.24), channel_id=1, source_target_pairs={{0,2},{2,0},{4,6},{6,4},{1,3},{3,1},{5,7},{7,5}} | collective-permute-start | bytes 1769480 | tf_op jit(solution)/shard_map/ppermute | solution.py:24
  1113.7 85.9 %collective-permute-start.25 = (f32[512,1536]{1,0:T(8,128)}, f32[512,1536]{1,0:T(8,128)}, u32[]{:S(2)}, u32[]{:S(2)}) collective-permute-start(f32[512,1536]{1,0:T(8,128)} %get-tuple-element.106), channel_id=1, source_target_pairs={{0,1},{1,0},{2,3},{3,2},{4,5},{5,4},{6,7},{7,6}} | collective-permute-start | bytes 9437192 | tf_op jit(solution)/shard_map/ppermute | solution.py:32
  1115.8 28.2 %collective-permute-start.50 = (f32[384,384]{0,1:T(8,128)S(1)}, f32[384,384]{0,1:T(8,128)S(1)}, u32[]{:S(2)}, u32[]{:S(2)}) collective-permute-start(f32[384,384]{0,1:T(8,128)S(1)} %fusion.55), channel_id=1, source_target_pairs={{0,1},{1,0},{2,3},{3,2},{4,5},{5,4},{6,7},{7,6}} | collective-permute-start | bytes 1769480 | tf_op jit(solution)/shard_map/ppermute | solution.py:32
  1116.5 27.8 %collective-permute-start.52 = (f32[384,384]{0,1:T(8,128)S(1)}, f32[384,384]{0,1:T(8,128)S(1)}, u32[]{:S(2)}, u32[]{:S(2)}) collective-permute-start(f32[384,384]{0,1:T(8,128)S(1)} %fusion.53), channel_id=1, source_target_pairs={{0,1},{1,0},{2,3},{3,2},{4,5},{5,4},{6,7},{7,6}} | collective-permute-start | bytes 1769480 | tf_op jit(solution)/shard_map/ppermute | solution.py:32
  1139.6 27.6 %collective-permute-start.54 = (f32[384,384]{0,1:T(8,128)S(1)}, f32[384,384]{0,1:T(8,128)S(1)}, u32[]{:S(2)}, u32[]{:S(2)}) collective-permute-start(f32[384,384]{0,1:T(8,128)S(1)} %convolution_add_fusion.20), channel_id=1, source_target_pairs={{0,4},{4,0},{2,6},{6,2},{1,5},{5,1},{3,7},{7,3}} | collective-permute-start | bytes 1769480 | tf_op jit(solution)/shard_map/ppermute | solution.py:28
  1144.0 28.1 %collective-permute-start.42 = (f32[384,384]{0,1:T(8,128)S(1)}, f32[384,384]{0,1:T(8,128)S(1)}, u32[]{:S(2)}, u32[]{:S(2)}) collective-permute-start(f32[384,384]{0,1:T(8,128)S(1)} %fusion.69), channel_id=1, source_target_pairs={{0,1},{1,0},{2,3},{3,2},{4,5},{5,4},{6,7},{7,6}} | collective-permute-start | bytes 1769480 | tf_op jit(solution)/shard_map/ppermute | solution.py:32
  1144.3 28.7 %collective-permute-start.44 = (f32[384,384]{0,1:T(8,128)S(1)}, f32[384,384]{0,1:T(8,128)S(1)}, u32[]{:S(2)}, u32[]{:S(2)}) collective-permute-start(f32[384,384]{0,1:T(8,128)S(1)} %convolution_add_fusion.26), channel_id=1, source_target_pairs={{0,2},{2,0},{4,6},{6,4},{1,3},{3,1},{5,7},{7,5}} | collective-permute-start | bytes 1769480 | tf_op jit(solution)/shard_map/ppermute | solution.py:24
  1167.3 21.0 %collective-permute-start.48 = (f32[384,384]{0,1:T(8,128)S(1)}, f32[384,384]{0,1:T(8,128)S(1)}, u32[]{:S(2)}, u32[]{:S(2)}) collective-permute-start(f32[384,384]{0,1:T(8,128)S(1)} %fusion.47), channel_id=1, source_target_pairs={{0,4},{4,0},{2,6},{6,2},{1,5},{5,1},{3,7},{7,3}} | collective-permute-start | bytes 1769480 | tf_op jit(solution)/shard_map/ppermute | solution.py:28
  1222.0 42.3 %collective-permute-start.60 = (bf16[512,1536]{1,0:T(8,128)(2,1)}, bf16[512,1536]{1,0:T(8,128)(2,1)}, u32[]{:S(2)}, u32[]{:S(2)}) collective-permute-start(bf16[512,1536]{1,0:T(8,128)(2,1)} %get-tuple-element.130), channel_id=1, source_target_pairs={{0,1},{1,0},{2,3},{3,2},{4,5},{5,4},{6,7},{7,6}} | collective-permute-start | bytes 4718600 | tf_op jit(solution)/shard_map/ppermute | solution.py:32
  1238.9 27.6 %collective-permute-start.30 = (f32[384,1152]{1,0:T(8,128)S(1)}, f32[384,1152]{1,0:T(8,128)S(1)}, u32[]{:S(2)}, u32[]{:S(2)}) collective-permute-start(f32[384,1152]{1,0:T(8,128)S(1)} %fusion.87), channel_id=1, source_target_pairs={{0,1},{1,0},{2,3},{3,2},{4,5},{5,4},{6,7},{7,6}} | collective-permute-start | bytes 5308424 | tf_op jit(solution)/shard_map/ppermute | solution.py:32
  1242.6 33.3 %collective-permute-start.37 = (f32[384,1152]{1,0:T(8,128)}, f32[384,1152]{1,0:T(8,128)S(1)}, u32[]{:S(2)}, u32[]{:S(2)}) collective-permute-start(f32[384,1152]{1,0:T(8,128)} %fusion.75), channel_id=1, source_target_pairs={{0,1},{1,0},{2,3},{3,2},{4,5},{5,4},{6,7},{7,6}} | collective-permute-start | bytes 5308424 | tf_op jit(solution)/shard_map/ppermute | solution.py:32
  1260.4 17.8 %collective-permute-start.27 = (f32[384,1152]{1,0:T(8,128)}, f32[384,1152]{1,0:T(8,128)S(1)}, u32[]{:S(2)}, u32[]{:S(2)}) collective-permute-start(f32[384,1152]{1,0:T(8,128)} %fusion.91), channel_id=1, source_target_pairs={{0,1},{1,0},{2,3},{3,2},{4,5},{5,4},{6,7},{7,6}} | collective-permute-start | bytes 5308424 | tf_op jit(solution)/shard_map/ppermute | solution.py:32
  1260.6 17.6 %collective-permute-start.29 = (f32[384,1152]{1,0:T(8,128)}, f32[384,1152]{1,0:T(8,128)}, u32[]{:S(2)}, u32[]{:S(2)}) collective-permute-start(f32[384,1152]{1,0:T(8,128)} %fusion.89), channel_id=1, source_target_pairs={{0,1},{1,0},{2,3},{3,2},{4,5},{5,4},{6,7},{7,6}} | collective-permute-start | bytes 5308424 | tf_op jit(solution)/shard_map/ppermute | solution.py:32
  1264.4 9.1 collective-permute-start.49
  1266.5 17.0 collective-permute-start.34
  1273.5 196.5 %collective-permute-start.61 = (bf16[1024,1536]{1,0:T(8,128)(2,1)S(1)}, bf16[1024,1536]{1,0:T(8,128)(2,1)S(1)}, u32[]{:S(2)}, u32[]{:S(2)}) collective-permute-start(bf16[1024,1536]{1,0:T(8,128)(2,1)S(1)} %constant_dynamic-update-slice_fusion), channel_id=1, source_target_pairs={{0,4},{2,6},{5,1},{7,3}} | collective-permute-start | bytes 9437192 | tf_op jit(solution)/shard_map/ppermute | solution.py:449
  1275.8 52.0 %collective-permute-start.31 = (f32[384,1152]{1,0:T(8,128)S(1)}, f32[384,1152]{1,0:T(8,128)}, u32[]{:S(2)}, u32[]{:S(2)}) collective-permute-start(f32[384,1152]{1,0:T(8,128)S(1)} %convolution_add_fusion.16), channel_id=1, source_target_pairs={{0,2},{2,0},{4,6},{6,4},{1,3},{3,1},{5,7},{7,5}} | collective-permute-start | bytes 5308424 | tf_op jit(solution)/shard_map/ppermute | solution.py:24
  1278.2 171.0 %collective-permute-start.36 = (f32[384,1152]{1,0:T(8,128)}, f32[384,1152]{1,0:T(8,128)S(1)}, u32[]{:S(2)}, u32[]{:S(2)}) collective-permute-start(f32[384,1152]{1,0:T(8,128)} %fusion.77), channel_id=1, source_target_pairs={{0,1},{1,0},{2,3},{3,2},{4,5},{5,4},{6,7},{7,6}} | collective-permute-start | bytes 5308424 | tf_op jit(solution)/shard_map/ppermute | solution.py:32
  1278.2 172.9 %collective-permute-start.38 = (f32[384,1152]{1,0:T(8,128)S(1)}, f32[384,1152]{1,0:T(8,128)S(1)}, u32[]{:S(2)}, u32[]{:S(2)}) collective-permute-start(f32[384,1152]{1,0:T(8,128)S(1)} %convolution_add_fusion.12), channel_id=1, source_target_pairs={{0,4},{4,0},{2,6},{6,2},{1,5},{5,1},{3,7},{7,3}} | collective-permute-start | bytes 5308424 | tf_op jit(solution)/shard_map/ppermute | solution.py:28
  1283.5 184.4 %collective-permute-start.26 = (f32[384,1152]{1,0:T(8,128)S(1)}, f32[384,1152]{1,0:T(8,128)S(1)}, u32[]{:S(2)}, u32[]{:S(2)}) collective-permute-start(f32[384,1152]{1,0:T(8,128)S(1)} %copy-done.104), channel_id=1, source_target_pairs={{0,1},{1,0},{2,3},{3,2},{4,5},{5,4},{6,7},{7,6}} | collective-permute-start | bytes 5308424 | tf_op jit(solution)/shard_map/ppermute | solution.py:32
  1327.8 121.3 %collective-permute-start.51 = (f32[384,384]{0,1:T(8,128)S(1)}, f32[384,384]{0,1:T(8,128)S(1)}, u32[]{:S(2)}, u32[]{:S(2)}) collective-permute-start(f32[384,384]{0,1:T(8,128)S(1)} %copy-done.109), channel_id=1, source_target_pairs={{0,4},{4,0},{2,6},{6,2},{1,5},{5,1},{3,7},{7,3}} | collective-permute-start | bytes 1769480 | tf_op jit(solution)/shard_map/ppermute | solution.py:28
  1449.1 18.5 %collective-permute-start.55 = (f32[384,384]{0,1:T(8,128)S(1)}, f32[384,384]{0,1:T(8,128)S(1)}, u32[]{:S(2)}, u32[]{:S(2)}) collective-permute-start(f32[384,384]{0,1:T(8,128)S(1)} %copy-done.108), channel_id=1, source_target_pairs={{0,2},{2,0},{4,6},{6,4},{1,3},{3,1},{5,7},{7,5}} | collective-permute-start | bytes 1769480 | tf_op jit(solution)/shard_map/ppermute | solution.py:24
  1449.1 84.6 %collective-permute-start.28 = (f32[384,1152]{1,0:T(8,128)}, f32[384,1152]{1,0:T(8,128)}, u32[]{:S(2)}, u32[]{:S(2)}) collective-permute-start(f32[384,1152]{1,0:T(8,128)} %convolution_add_fusion.18), channel_id=1, source_target_pairs={{0,2},{2,0},{4,6},{6,4},{1,3},{3,1},{5,7},{7,5}} | collective-permute-start | bytes 5308424 | tf_op jit(solution)/shard_map/ppermute | solution.py:24
  1451.2 83.0 %collective-permute-start.32 = (f32[384,1152]{1,0:T(8,128)}, f32[384,1152]{1,0:T(8,128)}, u32[]{:S(2)}, u32[]{:S(2)}) collective-permute-start(f32[384,1152]{1,0:T(8,128)} %fusion.26), channel_id=1, source_target_pairs={{0,4},{4,0},{2,6},{6,2},{1,5},{5,1},{3,7},{7,3}} | collective-permute-start | bytes 5308424 | tf_op jit(solution)/shard_map/ppermute | solution.py:28
  1467.7 72.3 %collective-permute-start.33 = (f32[384,1152]{1,0:T(8,128)}, f32[384,1152]{1,0:T(8,128)}, u32[]{:S(2)}, u32[]{:S(2)}) collective-permute-start(f32[384,1152]{1,0:T(8,128)} %fusion.81), channel_id=1, source_target_pairs={{0,1},{1,0},{2,3},{3,2},{4,5},{5,4},{6,7},{7,6}} | collective-permute-start | bytes 5308424 | tf_op jit(solution)/shard_map/ppermute | solution.py:32
  1467.9 122.3 %collective-permute-start.35 = (f32[384,1152]{1,0:T(8,128)}, f32[384,1152]{1,0:T(8,128)}, u32[]{:S(2)}, u32[]{:S(2)}) collective-permute-start(f32[384,1152]{1,0:T(8,128)} %convolution_add_fusion.14), channel_id=1, source_target_pairs={{0,4},{4,0},{2,6},{6,2},{1,5},{5,1},{3,7},{7,3}} | collective-permute-start | bytes 5308424 | tf_op jit(solution)/shard_map/ppermute | solution.py:28
  1470.0 124.2 %collective-permute-start.39 = (f32[384,1152]{1,0:T(8,128)}, f32[384,1152]{1,0:T(8,128)}, u32[]{:S(2)}, u32[]{:S(2)}) collective-permute-start(f32[384,1152]{1,0:T(8,128)} %fusion.23), channel_id=1, source_target_pairs={{0,2},{2,0},{4,6},{6,4},{1,3},{3,1},{5,7},{7,5}} | collective-permute-start | bytes 5308424 | tf_op jit(solution)/shard_map/ppermute | solution.py:24
  1533.7 68.4 %collective-permute-start.56 = (f32[384,384]{0,1:T(8,128)}, f32[384,384]{0,1:T(8,128)S(1)}, u32[]{:S(2)}, u32[]{:S(2)}) collective-permute-start(f32[384,384]{0,1:T(8,128)} %fusion.49), channel_id=1, source_target_pairs={{0,1},{1,0},{2,3},{3,2},{4,5},{5,4},{6,7},{7,6}} | collective-permute-start | bytes 1769480 | tf_op jit(solution)/shard_map/ppermute | solution.py:32
  1534.1 68.4 %collective-permute-start.57 = (f32[384,384]{0,1:T(8,128)S(1)}, f32[384,384]{0,1:T(8,128)S(1)}, u32[]{:S(2)}, u32[]{:S(2)}) collective-permute-start(f32[384,384]{0,1:T(8,128)S(1)} %fusion.50), channel_id=1, source_target_pairs={{0,1},{1,0},{2,3},{3,2},{4,5},{5,4},{6,7},{7,6}} | collective-permute-start | bytes 1769480 | tf_op jit(solution)/shard_map/ppermute | solution.py:32
  1540.0 121.6 %collective-permute-start.62 = (bf16[1024,1536]{1,0:T(8,128)(2,1)}, bf16[1024,1536]{1,0:T(8,128)(2,1)}, u32[]{:S(2)}, u32[]{:S(2)}) collective-permute-start(bf16[1024,1536]{1,0:T(8,128)(2,1)} %get-tuple-element.128), channel_id=1, source_target_pairs={{0,2},{2,0},{4,6},{6,4},{1,3},{3,1},{5,7},{7,5}} | collective-permute-start | bytes 9437192 | tf_op jit(solution)/shard_map/ppermute | solution.py:24
  1590.1 21.9 %collective-permute-start.40 = (f32[384,1152]{1,0:T(8,128)}, f32[384,1152]{1,0:T(8,128)}, u32[]{:S(2)}, u32[]{:S(2)}) collective-permute-start(f32[384,1152]{1,0:T(8,128)} %fusion.28), channel_id=1, source_target_pairs={{0,1},{1,0},{2,3},{3,2},{4,5},{5,4},{6,7},{7,6}} | collective-permute-start | bytes 5308424 | tf_op jit(solution)/shard_map/ppermute | solution.py:32
  1594.2 83.1 %collective-permute-start.58 = (f32[768,1536]{1,0:T(8,128)}, f32[768,1536]{1,0:T(8,128)}, u32[]{:S(2)}, u32[]{:S(2)}) collective-permute-start(f32[768,1536]{1,0:T(8,128)} %reduce-scatter.3.cloned.1.call-done), channel_id=1, source_target_pairs={{0,1},{1,0},{2,3},{3,2},{4,5},{5,4},{6,7},{7,6}} | collective-permute-start | bytes 14155784 | tf_op jit(solution)/shard_map/ppermute | solution.py:32
  1602.1 9.9 collective-permute-start.41
  1602.5 89.4 %collective-permute-start.59 = (f32[768,1536]{1,0:T(8,128)}, f32[768,1536]{1,0:T(8,128)}, u32[]{:S(2)}, u32[]{:S(2)}) collective-permute-start(f32[768,1536]{1,0:T(8,128)} %reduce-scatter.5.cloned.1.call-done), channel_id=1, source_target_pairs={{0,1},{1,0},{2,3},{3,2},{4,5},{5,4},{6,7},{7,6}} | collective-permute-start | bytes 14155784 | tf_op jit(solution)/shard_map/ppermute | solution.py:32
  (163 other events, 2993.9 us)
Sparse Core Ops, SparseCore 0:
  10.4 49.3 all-gather.9
  62.1 52.3 all-gather.7
  116.9 42.2 all-gather.5
  160.9 33.2 all-gather.11
  196.4 93.0 all-gather.13
  998.6 242.5 reduce-scatter.2
  1244.8 336.0 reduce-scatter.4

commit v4 on v3

--- a/solution.py
+++ b/solution.py
@@ -184,14 +184,12 @@
 
 GELU_C = 0.7978845608028654
 GELU_A = 0.044715
-BLOCK_F = 1024
-SUB_F = 512
+BLOCK_F = 768
+SUB_F = 768
 ROWS = (slice(0, 256), slice(256, 512))
 
 
-def mlp_fwd_body(*refs):
-    m_ref, h_ref, w1_ref, w2_ref = refs[:4]
-    z_ref, g_ref, x_ref, acc_ref = refs[-4:]
+def mlp_fwd_body(m_ref, h_ref, w1_ref, w2_ref, z_ref, g_ref, x_ref, acc_ref):
     j = pl.program_id(0)
 
     @pl.when(j == 0)
@@ -215,28 +213,26 @@
         x_ref[...] = acc_ref[...].astype(BF16)
 
 
-def mlp_fwd(m, h, w1t, w2, layer, layers, hist):
+def mlp_fwd(m, h, w1t, w2):
     t, dim = m.shape
     hidden = w2.shape[0]
     whole = pl.BlockSpec((t, dim), lambda j: (0, 0))
     wblk = pl.BlockSpec((BLOCK_F, dim), lambda j: (j, 0))
-    hspec = pl.BlockSpec((1, t, BLOCK_F), lambda j: (layer, 0, j))
-    extra = [] if hist is None else [hist]
     return pl.pallas_call(
         mlp_fwd_body,
         grid=(hidden // BLOCK_F,),
-        in_specs=[whole, whole, wblk, wblk] + [pl.BlockSpec(memory_space=pl.ANY)] * len(extra),
-        out_specs=[pl.BlockSpec((t, BLOCK_F), lambda j: (0, j)), hspec, whole],
+        in_specs=[whole, whole, wblk, wblk],
+        out_specs=[pl.BlockSpec((t, BLOCK_F), lambda j: (0, j)),
+                   pl.BlockSpec((1, t, BLOCK_F), lambda j: (j, 0, 0)), whole],
         out_shape=[jax.ShapeDtypeStruct((t, hidden), BF16),
-                   jax.ShapeDtypeStruct((layers, t, hidden), BF16),
+                   jax.ShapeDtypeStruct((hidden // BLOCK_F, t, BLOCK_F), BF16),
                    jax.ShapeDtypeStruct((t, dim), BF16)],
         scratch_shapes=[pltpu.VMEM((t, dim), F32)],
-        input_output_aliases={4: 1} if extra else {},
         compiler_params=pltpu.CompilerParams(dimension_semantics=('arbitrary',), vmem_limit_bytes=48 * 1024 * 1024),
         cost_estimate=pl.CostEstimate(flops=4 * t * dim * hidden, bytes_accessed=4 * dim * hidden + 4 * t * hidden,
                                       transcendentals=t * hidden),
         name='mlp_fwd',
-    )(m, h, w1t, w2, *extra)
+    )(m, h, w1t, w2)
 
 
 def mlp_bwd_body(*refs):
@@ -382,7 +378,8 @@
         d_cur = my_tokens(cot_out)
 
         saved = []
-        g_hist = u_hist = m_hist = ctx_hist = None
+        g_mine = []
+        u_hist = m_hist = ctx_hist = None
         for layer in range(layer_count):
             s = x_cur.astype(F32) + step_emb[layer].astype(F32)
             u = rms_norm(s).astype(BF16)
@@ -392,7 +389,8 @@
             ctx, lse = attn_fwd(q, kv, kv_s)
             h = (s + nn(ctx, wo)).astype(BF16)
             m = rms_norm(h.astype(F32)).astype(BF16)
-            z, g_hist, x_next = mlp_fwd(m, h, w1, w2, layer, layer_count, g_hist)
+            z, g, x_next = mlp_fwd(m, h, w1, w2)
+            g_mine.append(lax.all_to_all(g.reshape(-1, g.shape[-1]), BOTH, split_axis=0, concat_axis=0, tiled=True))
             u_hist, m_hist, ctx_hist = keep(u_hist, u, layer), keep(m_hist, m, layer), keep(ctx_hist, ctx, layer)
             saved.append((x_cur, q, kv, kv_s, lse, h, z))
             x_cur = x_next
@@ -400,14 +398,13 @@
         def flat(v):
             return v.reshape(-1, v.shape[-1])
 
-        up_hist = next_hist = mid_hist = dq_hist = dkv_hist = None
+        up_hist = mid_hist = dq_hist = dkv_hist = grad_2 = None
         for layer in reversed(range(layer_count)):
             x_l, q, kv, kv_s, lse, h, z = saved[layer]
             d_next = d_cur
-            next_hist = keep(next_hist, d_next, layer)
-            if layer == 0:
-                term_2, d_next = lax.optimization_barrier((tn(flat(g_hist), flat(next_hist)), d_next))
-                grad_2 = scatter(term_2)
+            next_all = gather(d_next)
+            term = tn(g_mine[layer], next_all)
+            grad_2 = term if grad_2 is None else grad_2 + term
             up_hist, d_mid = mlp_bwd(d_next, h, z, w1, w2, layer, layer_count, up_hist)
             mid_hist = keep(mid_hist, d_mid, layer)
             if layer == 0:
@@ -451,8 +448,11 @@
         d_x = jnp.zeros((2,) + whole.shape, BF16)
         d_x = put(put(d_x, row_seq[None], chip_x, 0), pp_x(row_seq)[None], 1 - chip_x, 0)
 
-        grad_1 = ordered(grad_1, pp_d(grad_1), 0).T
-        grad_2 = ordered(grad_2, pp_d(grad_2), 0)
+        def both_halves(v):
+            return lax.all_gather(v, 'data', axis=0, tiled=True)
+
+        grad_1 = both_halves(grad_1).T
+        grad_2 = both_halves(grad_2)
         return (grad_qkv[:, :hid], grad_qkv[:, hid:2 * hid], grad_qkv[:, 2 * hid:], grad_o, grad_1, grad_2, d_x)
 
     return jax.shard_map(device_step, mesh=mesh,

time: 1710 us -> 1790 us (1.047)
  waiting for transfers between devices: 574 us -> 605 us
  matrix products: 328 us -> 358 us
    all_to_all x0 -> x4, waiting for transfers between devices: none -> 235 us  [device_step(): lax.all_to_all(g.reshape(-1, g.shape[-1]), BOTH, split_axis=0, concat_axi...]
    ppermute x10, waiting for transfers between devices: 241 us -> 135 us  [pp_x(): return lax.ppermute(v, 'model', SWAP_X)]
    ppermute x9, waiting for transfers between devices: 223 us -> 122 us  [pp_y(): return lax.ppermute(v, 'model', SWAP_Y)]
    dot_general x66 -> x69, matrix products: 328 us -> 358 us  [dot(): return lax.dot_general(a, b, (dims, ((), ())), preferred_element_type=F32)]
    dynamic_update_slice x21 -> x17, local copies, waits for them, and re-layouts: 48 us -> 36.6 us  [put(): return lax.dynamic_update_slice_in_dim(buf, v, which * v.shape[axis], axis)]
    unnamed x319 -> x346, local copies, waits for them, and re-layouts: 53 us -> 49.1 us
    all_gather x5 -> x9, waiting for transfers between devices: 85.2 us -> 84.9 us  [gather(): return lax.all_gather(v, BOTH, axis=0, tiled=True)]
  transfers between devices with their start and end apart: 70 -> 77, of which waited for: 21 -> 24; matrix products, arithmetic and copies ran while one was open for 20% -> 27% of each run, Pallas kernels for 4% -> 14%
where the time goes in v4:
time: 1790 us
  waiting for transfers between devices  605 us (34%)
  Pallas kernels  520 us (29%)
  matrix products  358 us (20%)
  local copies, waits for them, and re-layouts  162 us (9%)
  other arithmetic  72.4 us (4%)
  starting transfers between devices  54.7 us (3%)
    dot_general x69, matrix products, dot(): return lax.dot_general(a, b, (dims, ((), ())), preferred_element_type=F32)  358 us
    all_to_all x4, waiting for transfers between devices, device_step(): lax.all_to_all(g.reshape(-1, g.shape[-1]), BOTH, split_axis=0, concat_axi...  235 us
    pallas_call x4, Pallas kernels, attn_bwd(): pl.pallas_call(attn_bwd_body, grid=(pairs,), in_specs=[pl.BlockSpec((tq,...  196 us
    ppermute x10, waiting for transfers between devices, pp_x(): return lax.ppermute(v, 'model', SWAP_X)  135 us
    ppermute x9, waiting for transfers between devices, pp_y(): return lax.ppermute(v, 'model', SWAP_Y)  122 us
    pallas_call x4, Pallas kernels, mlp_bwd(): pl.pallas_call(mlp_bwd_body, grid=(hidden // BLOCK_F,), in_specs=[whole,...  117 us
    pallas_call x4, Pallas kernels, mlp_fwd(): pl.pallas_call(mlp_fwd_body, grid=(hidden // BLOCK_F,), in_specs=[whole,...  112 us
    pallas_call x4, Pallas kernels, attn_fwd(): pl.pallas_call(attn_fwd_body, grid=(pairs,), in_specs=[pl.BlockSpec((tq,...  95.6 us
  transfers between devices with their start and end apart: 77, of which 24 were waited for; matrix products, arithmetic and copies ran while one was open for 27% of the time, Pallas kernels for 14%

profile of v4, /device:TPU:0, one launch (start us, length us, event | category | flops | bytes accessed | tf_op | source)
XLA Modules:
  0.0 1789.3 jit_solution(5380657147512444418)
XLA Ops:
  29.8 35.4 %collective-permute-done.2 = bf16[384,1536]{1,0:T(8,128)(2,1)} collective-permute-done((bf16[384,1536]{1,0:T(8,128)(2,1)}, bf16[384,1536]{1,0:T(8,128)(2,1)}, u32[]{:S(2)}, u32[]{:S(2)}) %collective-permute-start.2) | collective-permute-done | bytes 1179680 | tf_op jit(solution)/shard_map/ppermute | solution.py:24
  65.2 6.7 broadcast_in_dim.116
  82.2 23.6 %collective-permute-done.4 = bf16[384,1536]{1,0:T(8,128)(2,1)} collective-permute-done((bf16[384,1536]{1,0:T(8,128)(2,1)}, bf16[384,1536]{1,0:T(8,128)(2,1)}, u32[]{:S(2)}, u32[]{:S(2)}) %collective-permute-start.4) | collective-permute-done | bytes 1179680 | tf_op jit(solution)/shard_map/ppermute | solution.py:24
  107.3 6.5 collective-permute-done.6
  121.7 5.2 convolution_convert_fusion.14
  131.6 16.2 collective-permute-done.10
  172.5 23.7 %attn_fwd.4 = (bf16[512,1536]{1,0:T(8,128)(2,1)S(1)}, f32[12,2,512]{2,1,0:T(2,128)S(1)}) custom-call(bf16[512,1536]{1,0:T(8,128)(2,1)S(1)} %convolution_convert_fusion.15.q_ref.refs_0_, bf16[512,3072]{1,0:T(8,128)(2,1)} %pad_maximum_fusion.4.ko_ref.vo_ref.refs_1_.refs_3_, bf16[512,3072]{1,0:T(8,128)(2,1)} %collective-permute-done.1.ks_ref.vs_ref.refs_2_.refs_4_, ...), custom_call_target="tpu_custom_call" | custom-call | flops 12884901888 | bytes 9437184 | tf_op jit(solution)/shard_map/attn_fwd/pallas_call | solution.py:95
  197.4 6.9 fusion
  204.6 84.8 %all-gather.20.cloned.1.call-done.w1_ref.refs_3_ = bf16[6144,1536]{1,0:T(8,128)(2,1)} async-done(((bf16[768,1536]{1,0:T(8,128)(2,1)}), bf16[6144,1536]{1,0:T(8,128)(2,1)}) %all-gather.20.cloned.1.call-update) | async-done | bytes 18874384 | tf_op jit(solution)/shard_map/all_gather | solution.py:342
  289.5 27.0 %mlp_fwd.4 = (bf16[512,6144]{1,0:T(8,128)(2,1)}, bf16[8,512,768]{2,1,0:T(8,128)(2,1)}, bf16[512,1536]{1,0:T(8,128)(2,1)S(1)}) custom-call(bf16[512,1536]{1,0:T(8,128)(2,1)S(1)} %fusion.1.m_ref, bf16[512,1536]{1,0:T(8,128)(2,1)S(1)} %get-tuple-element.163.h_ref.refs_1_, bf16[6144,1536]{1,0:T(8,128)(2,1)} %all-gather.20.cloned.1.call-done.w1_ref.refs_3_, ...), custom_call_target="tpu_custom_call" | custom-call | flops 19327352832 | bytes 50331648 | tf_op jit(solution)/shard_map/mlp_fwd/pallas_call | solution.py:221
  333.6 24.4 %attn_fwd.5 = (bf16[512,1536]{1,0:T(8,128)(2,1)S(1)}, f32[12,2,512]{2,1,0:T(2,128)S(1)}) custom-call(bf16[512,1536]{1,0:T(8,128)(2,1)S(1)} %convolution_convert_fusion.12.q_ref.refs_0_, bf16[512,3072]{1,0:T(8,128)(2,1)} %copy-done.76, bf16[512,3072]{1,0:T(8,128)(2,1)} %collective-permute-done.14.ks_ref.vs_ref.refs_2_.refs_4_, bf16[512,3072]{1,0:T(8,128)(2,1)} %copy-done.76, ...), custom_call_target="tpu_custom_call" | custom-call | flops 12884901888 | bytes 9437184 | tf_op jit(solution)/shard_map/attn_fwd/pallas_call | solution.py:95
  358.0 5.6 fusion.2
  364.0 27.3 %mlp_fwd.5 = (bf16[512,6144]{1,0:T(8,128)(2,1)}, bf16[8,512,768]{2,1,0:T(8,128)(2,1)}, bf16[512,1536]{1,0:T(8,128)(2,1)S(1)}) custom-call(bf16[512,1536]{1,0:T(8,128)(2,1)S(1)} %get-tuple-element.132.m_ref, bf16[512,1536]{1,0:T(8,128)(2,1)S(1)} %get-tuple-element.165.h_ref.refs_1_, bf16[6144,1536]{1,0:T(8,128)(2,1)} %all-gather.20.cloned.1.call-done.w1_ref.refs_3_, ...), custom_call_target="tpu_custom_call" | custom-call | flops 19327352832 | bytes 50331648 | tf_op jit(solution)/shard_map/mlp_fwd/pallas_call | solution.py:221
  408.3 23.7 %attn_fwd.6 = (bf16[512,1536]{1,0:T(8,128)(2,1)S(1)}, f32[12,2,512]{2,1,0:T(2,128)S(1)}) custom-call(bf16[512,1536]{1,0:T(8,128)(2,1)S(1)} %convolution_convert_fusion.9.q_ref.refs_0_, bf16[512,3072]{1,0:T(8,128)(2,1)} %copy-done.77, bf16[512,3072]{1,0:T(8,128)(2,1)} %collective-permute-done.15.ks_ref.vs_ref.refs_2_.refs_4_, bf16[512,3072]{1,0:T(8,128)(2,1)} %copy-done.77, ...), custom_call_target="tpu_custom_call" | custom-call | flops 12884901888 | bytes 9437184 | tf_op jit(solution)/shard_map/attn_fwd/pallas_call | solution.py:95
  432.0 5.6 fusion.4
  438.0 29.9 %mlp_fwd.6 = (bf16[512,6144]{1,0:T(8,128)(2,1)}, bf16[8,512,768]{2,1,0:T(8,128)(2,1)}, bf16[512,1536]{1,0:T(8,128)(2,1)S(1)}) custom-call(bf16[512,1536]{1,0:T(8,128)(2,1)S(1)} %get-tuple-element.130.m_ref, bf16[512,1536]{1,0:T(8,128)(2,1)S(1)} %get-tuple-element.167.h_ref.refs_1_, bf16[6144,1536]{1,0:T(8,128)(2,1)} %all-gather.20.cloned.1.call-done.w1_ref.refs_3_, ...), custom_call_target="tpu_custom_call" | custom-call | flops 19327352832 | bytes 50331648 | tf_op jit(solution)/shard_map/mlp_fwd/pallas_call | solution.py:221
  481.8 7.2 collective-permute-done.16
  489.6 5.6 convolution_convert_fusion.6.q_ref.refs_0_
  495.3 23.8 %attn_fwd.7 = (bf16[512,1536]{1,0:T(8,128)(2,1)S(1)}, f32[12,2,512]{2,1,0:T(2,128)S(1)}) custom-call(bf16[512,1536]{1,0:T(8,128)(2,1)S(1)} %convolution_convert_fusion.6.q_ref.refs_0_, bf16[512,3072]{1,0:T(8,128)(2,1)} %pad_maximum_fusion.7.ko_ref.vo_ref.refs_1_.refs_3_, bf16[512,3072]{1,0:T(8,128)(2,1)} %collective-permute-done.17.ks_ref.vs_ref.refs_2_.refs_4_, ...), custom_call_target="tpu_custom_call" | custom-call | flops 12884901888 | bytes 9437184 | tf_op jit(solution)/shard_map/attn_fwd/pallas_call | solution.py:95
  523.3 27.7 %mlp_fwd.7 = (bf16[512,6144]{1,0:T(8,128)(2,1)}, bf16[8,512,768]{2,1,0:T(8,128)(2,1)}, bf16[512,1536]{1,0:T(8,128)(2,1)}) custom-call(bf16[512,1536]{1,0:T(8,128)(2,1)S(1)} %get-tuple-element.128.m_ref, bf16[512,1536]{1,0:T(8,128)(2,1)S(1)} %get-tuple-element.169.h_ref.refs_1_, bf16[6144,1536]{1,0:T(8,128)(2,1)} %all-gather.20.cloned.1.call-done.w1_ref.refs_3_, ...), custom_call_target="tpu_custom_call" | custom-call | flops 19327352832 | bytes 50331648 | tf_op jit(solution)/shard_map/mlp_fwd/pallas_call | solution.py:221
  551.0 29.1 %mlp_bwd.4 = (bf16[4,512,6144]{2,1,0:T(8,128)(2,1)}, bf16[512,1536]{1,0:T(8,128)(2,1)S(1)}) custom-call(bf16[512,1536]{1,0:T(8,128)(2,1)S(1)} %bitcast_select_fusion.refs_0_, bf16[512,1536]{1,0:T(8,128)(2,1)S(1)} %get-tuple-element.169.h_ref.refs_1_, bf16[512,6144]{1,0:T(8,128)(2,1)} %get-tuple-element.63.refs_2_, ...), custom_call_target="tpu_custom_call" | custom-call | flops 19327352832 | bytes 50331648 | tf_op jit(solution)/shard_map/mlp_bwd/pallas_call | solution.py:275
  582.8 48.9 %attn_bwd.4 = (bf16[4,512,1536]{2,1,0:T(8,128)(2,1)}, f32[512,1536]{1,0:T(8,128)}, f32[512,1536]{1,0:T(8,128)}, f32[512,1536]{1,0:T(8,128)}, f32[512,1536]{1,0:T(8,128)}) custom-call(bf16[512,1536]{1,0:T(8,128)(2,1)S(1)} %convolution_convert_fusion.6.q_ref.refs_0_, bf16[512,3072]{1,0:T(8,128)(2,1)} %pad_maximum_fusion.7.ko_ref.vo_ref.refs_1_.refs_3_, ...), custom_call_target="tpu_custom_call" | custom-call | flops 32212254720 | bytes 25165824 | tf_op jit(solution)/shard_map/attn_bwd/pallas_call | solution.py:164
  632.2 5.4 collective-permute-done.18
  640.1 5.5 fusion.109
  657.1 29.3 %mlp_bwd.5 = (bf16[4,512,6144]{2,1,0:T(8,128)(2,1)}, bf16[512,1536]{1,0:T(8,128)(2,1)S(1)}) custom-call(bf16[512,1536]{1,0:T(8,128)(2,1)S(1)} %copy-done.10, bf16[512,1536]{1,0:T(8,128)(2,1)S(1)} %copy-done.27, bf16[512,6144]{1,0:T(8,128)(2,1)} %get-tuple-element.71.refs_2_, ...), custom_call_target="tpu_custom_call", output_to_operand_aliasing={{0}: (5, {})} | custom-call | flops 19327352832 | bytes 50331648 | tf_op jit(solution)/shard_map/mlp_bwd/pallas_call | solution.py:275
  686.4 5.6 convolution_convert_fusion.2.refs_5_
  692.0 48.9 %attn_bwd.5 = (bf16[4,512,1536]{2,1,0:T(8,128)(2,1)}, f32[512,1536]{1,0:T(8,128)}, f32[512,1536]{1,0:T(8,128)}, f32[512,1536]{1,0:T(8,128)}, f32[512,1536]{1,0:T(8,128)}) custom-call(bf16[512,1536]{1,0:T(8,128)(2,1)S(1)} %copy-done.41, bf16[512,3072]{1,0:T(8,128)(2,1)} %copy-done.77, ...), custom_call_target="tpu_custom_call", output_to_operand_aliasing={{0}: (7, {})} | custom-call | flops 32212254720 | bytes 25165824 | tf_op jit(solution)/shard_map/attn_bwd/pallas_call | solution.py:164
  741.4 5.4 collective-permute-done.20
  749.3 5.2 fusion.110
  766.6 29.2 %mlp_bwd.6 = (bf16[4,512,6144]{2,1,0:T(8,128)(2,1)}, bf16[512,1536]{1,0:T(8,128)(2,1)S(1)}) custom-call(bf16[512,1536]{1,0:T(8,128)(2,1)S(1)} %copy-done.11, bf16[512,1536]{1,0:T(8,128)(2,1)S(1)} %copy-done.25, bf16[512,6144]{1,0:T(8,128)(2,1)} %get-tuple-element.80.refs_2_, ...), custom_call_target="tpu_custom_call", output_to_operand_aliasing={{0}: (5, {})} | custom-call | flops 19327352832 | bytes 50331648 | tf_op jit(solution)/shard_map/mlp_bwd/pallas_call | solution.py:275
  795.8 5.6 convolution_convert_fusion.1.refs_5_
  801.4 48.8 %attn_bwd.6 = (bf16[4,512,1536]{2,1,0:T(8,128)(2,1)}, f32[512,1536]{1,0:T(8,128)}, f32[512,1536]{1,0:T(8,128)}, f32[512,1536]{1,0:T(8,128)}, f32[512,1536]{1,0:T(8,128)}) custom-call(bf16[512,1536]{1,0:T(8,128)(2,1)S(1)} %copy-done.39, bf16[512,3072]{1,0:T(8,128)(2,1)} %copy-done.76, ...), custom_call_target="tpu_custom_call", output_to_operand_aliasing={{0}: (7, {})} | custom-call | flops 32212254720 | bytes 25165824 | tf_op jit(solution)/shard_map/attn_bwd/pallas_call | solution.py:164
  850.7 5.4 collective-permute-done.22
  858.6 5.5 fusion.111
  876.4 29.1 %mlp_bwd.7 = (bf16[4,512,6144]{2,1,0:T(8,128)(2,1)}, bf16[512,1536]{1,0:T(8,128)(2,1)S(1)}) custom-call(bf16[512,1536]{1,0:T(8,128)(2,1)S(1)} %copy-done.12, bf16[512,1536]{1,0:T(8,128)(2,1)S(1)} %copy-done.14, bf16[512,6144]{1,0:T(8,128)(2,1)} %get-tuple-element.89.refs_2_, ...), custom_call_target="tpu_custom_call", output_to_operand_aliasing={{0}: (5, {})} | custom-call | flops 19327352832 | bytes 50331648 | tf_op jit(solution)/shard_map/mlp_bwd/pallas_call | solution.py:275
  906.6 47.2 %convolution_bitcast_fusion = f32[6144,1536]{1,0:T(8,128)} fusion(bf16[4,512,6144]{2,1,0:T(8,128)(2,1)} %get-tuple-element.91, bf16[4,512,1536]{2,1,0:T(8,128)(2,1)} %get-tuple-element.127), kind=kOutput, calls=%fused_computation | convolution fusion | flops 38654705664 | bytes 69206016 | tf_op jit(solution)/shard_map/dot_general | solution.py:40
  973.4 49.1 %attn_bwd.7 = (bf16[4,512,1536]{2,1,0:T(8,128)(2,1)}, f32[512,1536]{1,0:T(8,128)}, f32[512,1536]{1,0:T(8,128)}, f32[512,1536]{1,0:T(8,128)}, f32[512,1536]{1,0:T(8,128)}) custom-call(bf16[512,1536]{1,0:T(8,128)(2,1)S(1)} %copy-done.37, bf16[512,3072]{1,0:T(8,128)(2,1)} %pad_maximum_fusion.4.ko_ref.vo_ref.refs_1_.refs_3_, ...), custom_call_target="tpu_custom_call", output_to_operand_aliasing={{0}: (7, {})} | custom-call | flops 32212254720 | bytes 25165824 | tf_op jit(solution)/shard_map/attn_bwd/pallas_call | solution.py:164
  1025.0 8.2 dynamic_update_slice.144
  1040.4 7.2 constant_dynamic-slice_fusion.6
  1049.8 21.2 %all-to-all-done.3 = bf16[8,512,768]{2,1,0:T(8,128)(2,1)} async-done(((bf16[8,512,768]{2,1,0:T(8,128)(2,1)}), bf16[8,512,768]{2,1,0:T(8,128)(2,1)}, u32[]{:S(2)}, u32[]{:S(2)}) %all-to-all-start.3) | async-done | bytes 6291488 | tf_op jit(solution)/shard_map/all_to_all | solution.py:393
  1080.1 5.6 fusion.115
  1089.0 5.5 convolution_add_fusion.1
  1107.2 50.6 %all-to-all-done.2 = bf16[8,512,768]{2,1,0:T(8,128)(2,1)} async-done(((bf16[8,512,768]{2,1,0:T(8,128)(2,1)}), bf16[8,512,768]{2,1,0:T(8,128)(2,1)}, u32[]{:S(2)}, u32[]{:S(2)}) %all-to-all-start.2) | async-done | bytes 6291488 | tf_op jit(solution)/shard_map/all_to_all | solution.py:393
  1166.5 7.9 constant_dynamic-slice_fusion.5
  1185.3 8.0 constant_dynamic-slice_fusion.18
  1198.2 96.5 %all-to-all-done.1 = bf16[8,512,768]{2,1,0:T(8,128)(2,1)} async-done(((bf16[8,512,768]{2,1,0:T(8,128)(2,1)}), bf16[8,512,768]{2,1,0:T(8,128)(2,1)}, u32[]{:S(2)}, u32[]{:S(2)}) %all-to-all-start.1) | async-done | bytes 6291488 | tf_op jit(solution)/shard_map/all_to_all | solution.py:393
  1299.3 17.3 fusion.112
  1316.6 16.3 fusion.113
  1333.0 16.5 fusion.114
  1349.4 66.5 %all-to-all-done = bf16[8,512,768]{2,1,0:T(8,128)(2,1)} async-done(((bf16[8,512,768]{2,1,0:T(8,128)(2,1)}), bf16[8,512,768]{2,1,0:T(8,128)(2,1)}, u32[]{:S(2)}, u32[]{:S(2)}) %all-to-all-start) | async-done | bytes 6291488 | tf_op jit(solution)/shard_map/all_to_all | solution.py:393
  1416.0 20.8 %add_add_fusion.4 = f32[768,1536]{1,0:T(8,128)} fusion(f32[768,1536]{1,0:T(8,128)} %fusion.114, f32[768,1536]{1,0:T(8,128)} %fusion.113, f32[768,1536]{1,0:T(8,128)} %fusion.112, bf16[4096,768]{1,0:T(8,128)(2,1)} %bitcast.38, bf16[4096,1536]{1,0:T(8,128)(2,1)} %all-gather.24.cloned.1.call-done), kind=kOutput, calls=%fused_computation.9 | convolution fusion | flops 9667215360 | bytes 37748736 | tf_op jit(solution)/shard_map/dot_general | solution.py:40
  1494.3 9.3 collective-permute-done.47
  1515.6 5.3 convolution_add_fusion.12
  1523.0 6.4 convolution_add_fusion.18
  1533.3 21.1 %collective-permute-done.31 = f32[384,1152]{1,0:T(8,128)S(1)} collective-permute-done((f32[384,1152]{1,0:T(8,128)}, f32[384,1152]{1,0:T(8,128)S(1)}, u32[]{:S(2)}, u32[]{:S(2)}) %collective-permute-start.31) | collective-permute-done | bytes 1769504 | tf_op jit(solution)/shard_map/ppermute | solution.py:24
  1560.1 29.2 %collective-permute-done.38 = f32[384,1152]{1,0:T(8,128)S(1)} collective-permute-done((f32[384,1152]{1,0:T(8,128)S(1)}, f32[384,1152]{1,0:T(8,128)S(1)}, u32[]{:S(2)}, u32[]{:S(2)}) %collective-permute-start.38) | collective-permute-done | bytes 1769504 | tf_op jit(solution)/shard_map/ppermute | solution.py:28
  1607.6 5.6 bitcast_dynamic-update-slice_fusion.1
  1613.3 23.7 %collective-permute-done.32 = f32[384,1152]{1,0:T(8,128)} collective-permute-done((f32[384,1152]{1,0:T(8,128)}, f32[384,1152]{1,0:T(8,128)}, u32[]{:S(2)}, u32[]{:S(2)}) %collective-permute-start.32) | collective-permute-done | bytes 1769504 | tf_op jit(solution)/shard_map/ppermute | solution.py:28
  1639.9 5.5 fusion.28
  1645.7 29.2 %collective-permute-done.35 = f32[384,1152]{1,0:T(8,128)S(1)} collective-permute-done((f32[384,1152]{1,0:T(8,128)S(1)}, f32[384,1152]{1,0:T(8,128)S(1)}, u32[]{:S(2)}, u32[]{:S(2)}) %collective-permute-start.35) | collective-permute-done | bytes 1769504 | tf_op jit(solution)/shard_map/ppermute | solution.py:28
  1684.3 12.4 collective-permute-done.48
  1715.4 45.1 %collective-permute-done.60 = bf16[1024,1536]{1,0:T(8,128)(2,1)} collective-permute-done((bf16[1024,1536]{1,0:T(8,128)(2,1)}, bf16[1024,1536]{1,0:T(8,128)(2,1)}, u32[]{:S(2)}, u32[]{:S(2)}) %collective-permute-start.60) | collective-permute-done | bytes 3145760 | tf_op jit(solution)/shard_map/ppermute | solution.py:24
  1764.2 9.6 copy.62
  1773.8 8.4 copy.125
  (655 shorter events, 393.4 us)
Async XLA Ops:
  7.2 109.5 %all-gather.16.cloned.1.call-start = ((), (), s32[]{:S(2)}) async-start(), calls=%async_computation.7 | async-start | bytes 5308416 | tf_op jit(solution)/shard_map/all_gather | solution.py:342
  9.9 111.8 %all-gather.14.cloned.1.call-start = ((), (), s32[]{:S(2)}) async-start(), calls=%async_computation.6 | async-start | bytes 5308416 | tf_op jit(solution)/shard_map/all_gather | solution.py:342
  11.4 156.1 %all-gather.12.cloned.1.call-start = ((), (), s32[]{:S(2)}) async-start(), calls=%async_computation.5 | async-start | bytes 5308416 | tf_op jit(solution)/shard_map/all_gather | solution.py:342
  12.9 184.5 %all-gather.18.cloned.1.call-start = ((), (), s32[]{:S(2)}) async-start(), calls=%async_computation.8 | async-start | bytes 5308416 | tf_op jit(solution)/shard_map/all_gather | solution.py:342
  13.8 275.6 %all-gather.20.cloned.1.call-start = ((), (), s32[]{:S(2)}) async-start(), calls=%async_computation.9 | async-start | bytes 21233664 | tf_op jit(solution)/shard_map/all_gather | solution.py:342
  18.2 1281.1 %all-gather.26.cloned.1.call-start = ((), (), s32[]{:S(2)}) async-start(), calls=%async_computation.13 | async-start | bytes 14155776 | tf_op jit(solution)/shard_map/all_gather | solution.py:342
  21.6 43.7 %collective-permute-start.2 = (bf16[384,1536]{1,0:T(8,128)(2,1)}, bf16[384,1536]{1,0:T(8,128)(2,1)}, u32[]{:S(2)}, u32[]{:S(2)}) collective-permute-start(bf16[384,1536]{1,0:T(8,128)(2,1)} %get-tuple-element.159), channel_id=1, source_target_pairs={{0,2},{2,0},{4,6},{6,4},{1,3},{3,1},{5,7},{7,5}} | collective-permute-start | bytes 3538952 | tf_op jit(solution)/shard_map/ppermute | solution.py:24
  27.8 51.4 %collective-permute-start = (bf16[512,1536]{1,0:T(8,128)(2,1)}, bf16[512,1536]{1,0:T(8,128)(2,1)S(1)}, u32[]{:S(2)}, u32[]{:S(2)}) collective-permute-start(bf16[512,1536]{1,0:T(8,128)(2,1)} %dynamic-slice_bitcast_fusion.1), channel_id=1, source_target_pairs={{0,1},{1,0},{2,3},{3,2},{4,5},{5,4},{6,7},{7,6}} | collective-permute-start | bytes 4718600 | tf_op jit(solution)/shard_map/ppermute | solution.py:32
  27.8 49.8 %collective-permute-start.8 = (bf16[384,1536]{1,0:T(8,128)(2,1)}, bf16[384,1536]{1,0:T(8,128)(2,1)}, u32[]{:S(2)}, u32[]{:S(2)}) collective-permute-start(bf16[384,1536]{1,0:T(8,128)(2,1)} %get-tuple-element.158), channel_id=1, source_target_pairs={{0,4},{4,0},{2,6},{6,2},{1,5},{5,1},{3,7},{7,3}} | collective-permute-start | bytes 3538952 | tf_op jit(solution)/shard_map/ppermute | solution.py:28
  29.3 76.5 %collective-permute-start.4 = (bf16[384,1536]{1,0:T(8,128)(2,1)}, bf16[384,1536]{1,0:T(8,128)(2,1)}, u32[]{:S(2)}, u32[]{:S(2)}) collective-permute-start(bf16[384,1536]{1,0:T(8,128)(2,1)} %get-tuple-element.158), channel_id=1, source_target_pairs={{0,2},{2,0},{4,6},{6,4},{1,3},{3,1},{5,7},{7,5}} | collective-permute-start | bytes 3538952 | tf_op jit(solution)/shard_map/ppermute | solution.py:24
  29.8 84.0 %collective-permute-start.6 = (bf16[384,1536]{1,0:T(8,128)(2,1)}, bf16[384,1536]{1,0:T(8,128)(2,1)}, u32[]{:S(2)}, u32[]{:S(2)}) collective-permute-start(bf16[384,1536]{1,0:T(8,128)(2,1)} %get-tuple-element.159), channel_id=1, source_target_pairs={{0,4},{4,0},{2,6},{6,2},{1,5},{5,1},{3,7},{7,3}} | collective-permute-start | bytes 3538952 | tf_op jit(solution)/shard_map/ppermute | solution.py:28
  65.2 48.6 %collective-permute-start.3 = (bf16[384,1536]{1,0:T(8,128)(2,1)}, bf16[384,1536]{1,0:T(8,128)(2,1)}, u32[]{:S(2)}, u32[]{:S(2)}) collective-permute-start(bf16[384,1536]{1,0:T(8,128)(2,1)} %collective-permute-done.2), channel_id=1, source_target_pairs={{0,1},{1,0},{2,3},{3,2},{4,5},{5,4},{6,7},{7,6}} | collective-permute-start | bytes 3538952 | tf_op jit(solution)/shard_map/ppermute | solution.py:32
  77.6 70.3 %collective-permute-start.10 = (bf16[384,1536]{1,0:T(8,128)(2,1)}, bf16[384,1536]{1,0:T(8,128)(2,1)}, u32[]{:S(2)}, u32[]{:S(2)}) collective-permute-start(bf16[384,1536]{1,0:T(8,128)(2,1)} %collective-permute-done.2), channel_id=1, source_target_pairs={{0,4},{4,0},{2,6},{6,2},{1,5},{5,1},{3,7},{7,3}} | collective-permute-start | bytes 3538952 | tf_op jit(solution)/shard_map/ppermute | solution.py:28
  79.1 78.8 %collective-permute-start.9 = (bf16[384,1536]{1,0:T(8,128)(2,1)}, bf16[384,1536]{1,0:T(8,128)(2,1)}, u32[]{:S(2)}, u32[]{:S(2)}) collective-permute-start(bf16[384,1536]{1,0:T(8,128)(2,1)} %collective-permute-done.8), channel_id=1, source_target_pairs={{0,1},{1,0},{2,3},{3,2},{4,5},{5,4},{6,7},{7,6}} | collective-permute-start | bytes 3538952 | tf_op jit(solution)/shard_map/ppermute | solution.py:32
  105.8 42.0 %collective-permute-start.12 = (bf16[384,1536]{1,0:T(8,128)(2,1)}, bf16[384,1536]{1,0:T(8,128)(2,1)}, u32[]{:S(2)}, u32[]{:S(2)}) collective-permute-start(bf16[384,1536]{1,0:T(8,128)(2,1)} %collective-permute-done.8), channel_id=1, source_target_pairs={{0,2},{2,0},{4,6},{6,4},{1,3},{3,1},{5,7},{7,5}} | collective-permute-start | bytes 3538952 | tf_op jit(solution)/shard_map/ppermute | solution.py:24
  113.8 15.3 collective-permute-start.5
  113.8 39.4 %collective-permute-start.7 = (bf16[384,1536]{1,0:T(8,128)(2,1)}, bf16[384,1536]{1,0:T(8,128)(2,1)}, u32[]{:S(2)}, u32[]{:S(2)}) collective-permute-start(bf16[384,1536]{1,0:T(8,128)(2,1)} %collective-permute-done.6), channel_id=1, source_target_pairs={{0,1},{1,0},{2,3},{3,2},{4,5},{5,4},{6,7},{7,6}} | collective-permute-start | bytes 3538952 | tf_op jit(solution)/shard_map/ppermute | solution.py:32
  129.1 43.4 %collective-permute-start.1 = (bf16[512,3072]{1,0:T(8,128)(2,1)}, bf16[512,3072]{1,0:T(8,128)(2,1)}, u32[]{:S(2)}, u32[]{:S(2)}) collective-permute-start(bf16[512,3072]{1,0:T(8,128)(2,1)} %pad_maximum_fusion.4.ko_ref.vo_ref.refs_1_.refs_3_), channel_id=1, source_target_pairs={{0,1},{1,0},{2,3},{3,2},{4,5},{5,4},{6,7},{7,6}} | collective-permute-start | bytes 9437192 | tf_op jit(solution)/shard_map/ppermute | solution.py:32
  147.8 15.0 collective-permute-start.11
  147.8 18.5 %collective-permute-start.13 = (bf16[384,1536]{1,0:T(8,128)(2,1)}, bf16[384,1536]{1,0:T(8,128)(2,1)S(1)}, u32[]{:S(2)}, u32[]{:S(2)}) collective-permute-start(bf16[384,1536]{1,0:T(8,128)(2,1)} %collective-permute-done.12), channel_id=1, source_target_pairs={{0,1},{1,0},{2,3},{3,2},{4,5},{5,4},{6,7},{7,6}} | collective-permute-start | bytes 3538952 | tf_op jit(solution)/shard_map/ppermute | solution.py:32
  480.9 14.3 collective-permute-start.17
  631.9 17.9 %collective-permute-start.19 = (f32[512,1536]{1,0:T(8,128)}, f32[512,1536]{1,0:T(8,128)S(1)}, u32[]{:S(2)}, u32[]{:S(2)}) collective-permute-start(f32[512,1536]{1,0:T(8,128)} %get-tuple-element.70), channel_id=1, source_target_pairs={{0,1},{1,0},{2,3},{3,2},{4,5},{5,4},{6,7},{7,6}} | collective-permute-start | bytes 9437192 | tf_op jit(solution)/shard_map/ppermute | solution.py:32
  655.6 661.0 %all-gather.28.cloned.1.call-start = ((), (), s32[]{:S(2)}) async-start(), calls=%async_computation.14 | async-start | bytes 14155776 | tf_op jit(solution)/shard_map/all_gather | solution.py:342
  765.1 567.9 %all-gather.30.cloned.1.call-start = ((), (), s32[]{:S(2)}) async-start(), calls=%async_computation.15 | async-start | bytes 14155776 | tf_op jit(solution)/shard_map/all_gather | solution.py:342
  874.5 474.9 %all-gather.24.cloned.1.call-start = ((), (), s32[]{:S(2)}) async-start(), calls=%async_computation.12 | async-start | bytes 14155776 | tf_op jit(solution)/shard_map/all_gather | solution.py:342
  875.2 640.0 %reduce-scatter.2.cloned.1.call-start = ((), (), s32[]{:S(2)}) async-start(), calls=%async_computation.10 | async-start | bytes 42467328 | tf_op jit(solution)/shard_map/reduce_scatter | solution.py:345
  958.4 112.5 %all-to-all-start.3 = ((bf16[8,512,768]{2,1,0:T(8,128)(2,1)}), bf16[8,512,768]{2,1,0:T(8,128)(2,1)}, u32[]{:S(2)}, u32[]{:S(2)}) async-start(bf16[8,512,768]{2,1,0:T(8,128)(2,1)} %get-tuple-element.104), calls=%async_computation.4 | async-start | bytes 12582912 | tf_op jit(solution)/shard_map/all_to_all | solution.py:393
  1022.4 53.4 %collective-permute-start.24 = (f32[512,1536]{1,0:T(8,128)}, f32[512,1536]{1,0:T(8,128)}, u32[]{:S(2)}, u32[]{:S(2)}) collective-permute-start(f32[512,1536]{1,0:T(8,128)} %get-tuple-element.97), channel_id=1, source_target_pairs={{0,1},{1,0},{2,3},{3,2},{4,5},{5,4},{6,7},{7,6}} | collective-permute-start | bytes 9437192 | tf_op jit(solution)/shard_map/ppermute | solution.py:32
  1036.5 49.3 %collective-permute-start.25 = (f32[512,1536]{1,0:T(8,128)}, f32[512,1536]{1,0:T(8,128)}, u32[]{:S(2)}, u32[]{:S(2)}) collective-permute-start(f32[512,1536]{1,0:T(8,128)} %get-tuple-element.99), channel_id=1, source_target_pairs={{0,1},{1,0},{2,3},{3,2},{4,5},{5,4},{6,7},{7,6}} | collective-permute-start | bytes 9437192 | tf_op jit(solution)/shard_map/ppermute | solution.py:32
  1070.9 86.9 %all-to-all-start.2 = ((bf16[8,512,768]{2,1,0:T(8,128)(2,1)}), bf16[8,512,768]{2,1,0:T(8,128)(2,1)}, u32[]{:S(2)}, u32[]{:S(2)}) async-start(bf16[8,512,768]{2,1,0:T(8,128)(2,1)} %get-tuple-element.103), calls=%async_computation.3 | async-start | bytes 12582912 | tf_op jit(solution)/shard_map/all_to_all | solution.py:393
  1102.7 402.8 %collective-permute-start.58 = (bf16[512,1536]{1,0:T(8,128)(2,1)}, bf16[512,1536]{1,0:T(8,128)(2,1)}, u32[]{:S(2)}, u32[]{:S(2)}) collective-permute-start(bf16[512,1536]{1,0:T(8,128)(2,1)} %get-tuple-element.126), channel_id=1, source_target_pairs={{0,1},{1,0},{2,3},{3,2},{4,5},{5,4},{6,7},{7,6}} | collective-permute-start | bytes 4718600 | tf_op jit(solution)/shard_map/ppermute | solution.py:32
  1157.8 136.9 %all-to-all-start.1 = ((bf16[8,512,768]{2,1,0:T(8,128)(2,1)}), bf16[8,512,768]{2,1,0:T(8,128)(2,1)}, u32[]{:S(2)}, u32[]{:S(2)}) async-start(bf16[8,512,768]{2,1,0:T(8,128)(2,1)} %get-tuple-element.102), calls=%async_computation.2 | async-start | bytes 12582912 | tf_op jit(solution)/shard_map/all_to_all | solution.py:393
  1176.2 306.0 %collective-permute-start.43 = (f32[384,384]{0,1:T(8,128)}, f32[384,384]{0,1:T(8,128)}, u32[]{:S(2)}, u32[]{:S(2)}) collective-permute-start(f32[384,384]{0,1:T(8,128)} %fusion.67), channel_id=1, source_target_pairs={{0,1},{1,0},{2,3},{3,2},{4,5},{5,4},{6,7},{7,6}} | collective-permute-start | bytes 1769480 | tf_op jit(solution)/shard_map/ppermute | solution.py:32
  1178.7 306.6 %collective-permute-start.46 = (f32[384,384]{0,1:T(8,128)}, f32[384,384]{0,1:T(8,128)}, u32[]{:S(2)}, u32[]{:S(2)}) collective-permute-start(f32[384,384]{0,1:T(8,128)} %fusion.63), channel_id=1, source_target_pairs={{0,1},{1,0},{2,3},{3,2},{4,5},{5,4},{6,7},{7,6}} | collective-permute-start | bytes 1769480 | tf_op jit(solution)/shard_map/ppermute | solution.py:32
  1180.9 306.9 %collective-permute-start.50 = (f32[384,384]{0,1:T(8,128)}, f32[384,384]{0,1:T(8,128)}, u32[]{:S(2)}, u32[]{:S(2)}) collective-permute-start(f32[384,384]{0,1:T(8,128)} %fusion.55), channel_id=1, source_target_pairs={{0,1},{1,0},{2,3},{3,2},{4,5},{5,4},{6,7},{7,6}} | collective-permute-start | bytes 1769480 | tf_op jit(solution)/shard_map/ppermute | solution.py:32
  1183.0 305.0 %collective-permute-start.53 = (f32[384,384]{0,1:T(8,128)}, f32[384,384]{0,1:T(8,128)}, u32[]{:S(2)}, u32[]{:S(2)}) collective-permute-start(f32[384,384]{0,1:T(8,128)} %fusion.51), channel_id=1, source_target_pairs={{0,1},{1,0},{2,3},{3,2},{4,5},{5,4},{6,7},{7,6}} | collective-permute-start | bytes 1769480 | tf_op jit(solution)/shard_map/ppermute | solution.py:32
  1294.7 121.3 %all-to-all-start = ((bf16[8,512,768]{2,1,0:T(8,128)(2,1)}), bf16[8,512,768]{2,1,0:T(8,128)(2,1)}, u32[]{:S(2)}, u32[]{:S(2)}) async-start(bf16[8,512,768]{2,1,0:T(8,128)(2,1)} %get-tuple-element.101), calls=%async_computation.1 | async-start | bytes 12582912 | tf_op jit(solution)/shard_map/all_to_all | solution.py:393
  1299.3 465.0 %all-gather.32.cloned.1.call-start = ((), (), s32[]{:S(2)}) async-start(), calls=%async_computation.16 | async-start | bytes 14155776 | tf_op jit(solution)/shard_map/all_gather | solution.py:452
  1436.8 327.5 %all-gather.22.cloned.1.call-start = ((), (), s32[]{:S(2)}) async-start(), calls=%async_computation.11 | async-start | bytes 14155776 | tf_op jit(solution)/shard_map/all_gather | solution.py:452
  1482.2 26.5 %collective-permute-start.30 = (f32[384,1152]{1,0:T(8,128)S(1)}, f32[384,1152]{1,0:T(8,128)S(1)}, u32[]{:S(2)}, u32[]{:S(2)}) collective-permute-start(f32[384,1152]{1,0:T(8,128)S(1)} %fusion.87), channel_id=1, source_target_pairs={{0,1},{1,0},{2,3},{3,2},{4,5},{5,4},{6,7},{7,6}} | collective-permute-start | bytes 5308424 | tf_op jit(solution)/shard_map/ppermute | solution.py:32
  1487.8 27.5 %collective-permute-start.37 = (f32[384,1152]{1,0:T(8,128)}, f32[384,1152]{1,0:T(8,128)}, u32[]{:S(2)}, u32[]{:S(2)}) collective-permute-start(f32[384,1152]{1,0:T(8,128)} %fusion.75), channel_id=1, source_target_pairs={{0,1},{1,0},{2,3},{3,2},{4,5},{5,4},{6,7},{7,6}} | collective-permute-start | bytes 5308424 | tf_op jit(solution)/shard_map/ppermute | solution.py:32
  1488.0 15.6 collective-permute-start.47
  1493.9 27.0 %collective-permute-start.27 = (f32[384,1152]{1,0:T(8,128)}, f32[384,1152]{1,0:T(8,128)}, u32[]{:S(2)}, u32[]{:S(2)}) collective-permute-start(f32[384,1152]{1,0:T(8,128)} %fusion.91), channel_id=1, source_target_pairs={{0,1},{1,0},{2,3},{3,2},{4,5},{5,4},{6,7},{7,6}} | collective-permute-start | bytes 5308424 | tf_op jit(solution)/shard_map/ppermute | solution.py:32
  1503.6 17.4 collective-permute-start.29
  1505.5 23.9 %collective-permute-start.34 = (f32[384,1152]{1,0:T(8,128)}, f32[384,1152]{1,0:T(8,128)}, u32[]{:S(2)}, u32[]{:S(2)}) collective-permute-start(f32[384,1152]{1,0:T(8,128)} %fusion.79), channel_id=1, source_target_pairs={{0,1},{1,0},{2,3},{3,2},{4,5},{5,4},{6,7},{7,6}} | collective-permute-start | bytes 5308424 | tf_op jit(solution)/shard_map/ppermute | solution.py:32
  1508.7 93.2 %collective-permute-start.59 = (bf16[1024,1536]{1,0:T(8,128)(2,1)}, bf16[1024,1536]{1,0:T(8,128)(2,1)}, u32[]{:S(2)}, u32[]{:S(2)}) collective-permute-start(bf16[1024,1536]{1,0:T(8,128)(2,1)} %constant_dynamic-update-slice_fusion), channel_id=1, source_target_pairs={{0,4},{2,6},{5,1},{7,3}} | collective-permute-start | bytes 9437192 | tf_op jit(solution)/shard_map/ppermute | solution.py:446
  1515.3 39.0 %collective-permute-start.31 = (f32[384,1152]{1,0:T(8,128)}, f32[384,1152]{1,0:T(8,128)S(1)}, u32[]{:S(2)}, u32[]{:S(2)}) collective-permute-start(f32[384,1152]{1,0:T(8,128)} %convolution_add_fusion.16), channel_id=1, source_target_pairs={{0,2},{2,0},{4,6},{6,4},{1,3},{3,1},{5,7},{7,5}} | collective-permute-start | bytes 5308424 | tf_op jit(solution)/shard_map/ppermute | solution.py:24
  1520.9 38.4 %collective-permute-start.36 = (f32[384,1152]{1,0:T(8,128)S(1)}, f32[384,1152]{1,0:T(8,128)S(1)}, u32[]{:S(2)}, u32[]{:S(2)}) collective-permute-start(f32[384,1152]{1,0:T(8,128)S(1)} %copy-done.123), channel_id=1, source_target_pairs={{0,1},{1,0},{2,3},{3,2},{4,5},{5,4},{6,7},{7,6}} | collective-permute-start | bytes 5308424 | tf_op jit(solution)/shard_map/ppermute | solution.py:32
  1521.0 68.3 %collective-permute-start.38 = (f32[384,1152]{1,0:T(8,128)S(1)}, f32[384,1152]{1,0:T(8,128)S(1)}, u32[]{:S(2)}, u32[]{:S(2)}) collective-permute-start(f32[384,1152]{1,0:T(8,128)S(1)} %convolution_add_fusion.12), channel_id=1, source_target_pairs={{0,4},{4,0},{2,6},{6,2},{1,5},{5,1},{3,7},{7,3}} | collective-permute-start | bytes 5308424 | tf_op jit(solution)/shard_map/ppermute | solution.py:28
  1529.4 72.6 %collective-permute-start.26 = (f32[384,1152]{1,0:T(8,128)S(1)}, f32[384,1152]{1,0:T(8,128)S(1)}, u32[]{:S(2)}, u32[]{:S(2)}) collective-permute-start(f32[384,1152]{1,0:T(8,128)S(1)} %copy-done.122), channel_id=1, source_target_pairs={{0,1},{1,0},{2,3},{3,2},{4,5},{5,4},{6,7},{7,6}} | collective-permute-start | bytes 5308424 | tf_op jit(solution)/shard_map/ppermute | solution.py:32
  1559.3 39.7 %collective-permute-start.54 = (f32[384,384]{0,1:T(8,128)S(1)}, f32[384,384]{0,1:T(8,128)S(1)}, u32[]{:S(2)}, u32[]{:S(2)}) collective-permute-start(f32[384,384]{0,1:T(8,128)S(1)} %copy-done.130), channel_id=1, source_target_pairs={{0,4},{4,0},{2,6},{6,2},{1,5},{5,1},{3,7},{7,3}} | collective-permute-start | bytes 1769480 | tf_op jit(solution)/shard_map/ppermute | solution.py:28
  1559.4 53.9 %collective-permute-start.28 = (f32[384,1152]{1,0:T(8,128)S(1)}, f32[384,1152]{1,0:T(8,128)}, u32[]{:S(2)}, u32[]{:S(2)}) collective-permute-start(f32[384,1152]{1,0:T(8,128)S(1)} %convolution_add_fusion.18), channel_id=1, source_target_pairs={{0,2},{2,0},{4,6},{6,4},{1,3},{3,1},{5,7},{7,5}} | collective-permute-start | bytes 5308424 | tf_op jit(solution)/shard_map/ppermute | solution.py:24
  1589.2 47.8 %collective-permute-start.32 = (f32[384,1152]{1,0:T(8,128)}, f32[384,1152]{1,0:T(8,128)}, u32[]{:S(2)}, u32[]{:S(2)}) collective-permute-start(f32[384,1152]{1,0:T(8,128)} %fusion.26), channel_id=1, source_target_pairs={{0,4},{4,0},{2,6},{6,2},{1,5},{5,1},{3,7},{7,3}} | collective-permute-start | bytes 5308424 | tf_op jit(solution)/shard_map/ppermute | solution.py:28
  1599.0 46.7 %collective-permute-start.33 = (f32[384,1152]{1,0:T(8,128)S(1)}, f32[384,1152]{1,0:T(8,128)S(1)}, u32[]{:S(2)}, u32[]{:S(2)}) collective-permute-start(f32[384,1152]{1,0:T(8,128)S(1)} %copy-done.121), channel_id=1, source_target_pairs={{0,1},{1,0},{2,3},{3,2},{4,5},{5,4},{6,7},{7,6}} | collective-permute-start | bytes 5308424 | tf_op jit(solution)/shard_map/ppermute | solution.py:32
  1602.0 72.9 %collective-permute-start.35 = (f32[384,1152]{1,0:T(8,128)S(1)}, f32[384,1152]{1,0:T(8,128)S(1)}, u32[]{:S(2)}, u32[]{:S(2)}) collective-permute-start(f32[384,1152]{1,0:T(8,128)S(1)} %convolution_add_fusion.14), channel_id=1, source_target_pairs={{0,4},{4,0},{2,6},{6,2},{1,5},{5,1},{3,7},{7,3}} | collective-permute-start | bytes 5308424 | tf_op jit(solution)/shard_map/ppermute | solution.py:28
  1602.0 75.4 %collective-permute-start.39 = (f32[384,1152]{1,0:T(8,128)S(1)}, f32[384,1152]{1,0:T(8,128)}, u32[]{:S(2)}, u32[]{:S(2)}) collective-permute-start(f32[384,1152]{1,0:T(8,128)S(1)} %fusion.23), channel_id=1, source_target_pairs={{0,2},{2,0},{4,6},{6,4},{1,3},{3,1},{5,7},{7,5}} | collective-permute-start | bytes 5308424 | tf_op jit(solution)/shard_map/ppermute | solution.py:24
  1613.3 32.1 %collective-permute-start.42 = (f32[384,384]{0,1:T(8,128)S(1)}, f32[384,384]{0,1:T(8,128)S(1)}, u32[]{:S(2)}, u32[]{:S(2)}) collective-permute-start(f32[384,384]{0,1:T(8,128)S(1)} %copy-done.127), channel_id=1, source_target_pairs={{0,1},{1,0},{2,3},{3,2},{4,5},{5,4},{6,7},{7,6}} | collective-permute-start | bytes 1769480 | tf_op jit(solution)/shard_map/ppermute | solution.py:32
  1637.0 45.5 %collective-permute-start.49 = (f32[384,384]{0,1:T(8,128)S(1)}, f32[384,384]{0,1:T(8,128)S(1)}, u32[]{:S(2)}, u32[]{:S(2)}) collective-permute-start(f32[384,384]{0,1:T(8,128)S(1)} %copy-done.124), channel_id=1, source_target_pairs={{0,1},{1,0},{2,3},{3,2},{4,5},{5,4},{6,7},{7,6}} | collective-permute-start | bytes 1769480 | tf_op jit(solution)/shard_map/ppermute | solution.py:32
  1645.4 38.9 %collective-permute-start.44 = (f32[384,384]{0,1:T(8,128)S(1)}, f32[384,384]{0,1:T(8,128)S(1)}, u32[]{:S(2)}, u32[]{:S(2)}) collective-permute-start(f32[384,384]{0,1:T(8,128)S(1)} %copy-done.125), channel_id=1, source_target_pairs={{0,2},{2,0},{4,6},{6,4},{1,3},{3,1},{5,7},{7,5}} | collective-permute-start | bytes 1769480 | tf_op jit(solution)/shard_map/ppermute | solution.py:24
  1645.7 54.3 %collective-permute-start.51 = (f32[384,384]{0,1:T(8,128)S(1)}, f32[384,384]{0,1:T(8,128)S(1)}, u32[]{:S(2)}, u32[]{:S(2)}) collective-permute-start(f32[384,384]{0,1:T(8,128)S(1)} %copy-done.126), channel_id=1, source_target_pairs={{0,4},{4,0},{2,6},{6,2},{1,5},{5,1},{3,7},{7,3}} | collective-permute-start | bytes 1769480 | tf_op jit(solution)/shard_map/ppermute | solution.py:28
  1674.9 21.8 %collective-permute-start.48 = (f32[384,384]{0,1:T(8,128)S(1)}, f32[384,384]{0,1:T(8,128)S(1)}, u32[]{:S(2)}, u32[]{:S(2)}) collective-permute-start(f32[384,384]{0,1:T(8,128)S(1)} %copy-done.128), channel_id=1, source_target_pairs={{0,4},{4,0},{2,6},{6,2},{1,5},{5,1},{3,7},{7,3}} | collective-permute-start | bytes 1769480 | tf_op jit(solution)/shard_map/ppermute | solution.py:28
  1677.3 22.7 %collective-permute-start.55 = (f32[384,384]{0,1:T(8,128)S(1)}, f32[384,384]{0,1:T(8,128)S(1)}, u32[]{:S(2)}, u32[]{:S(2)}) collective-permute-start(f32[384,384]{0,1:T(8,128)S(1)} %copy-done.131), channel_id=1, source_target_pairs={{0,2},{2,0},{4,6},{6,4},{1,3},{3,1},{5,7},{7,5}} | collective-permute-start | bytes 1769480 | tf_op jit(solution)/shard_map/ppermute | solution.py:24
  1682.6 77.9 %collective-permute-start.60 = (bf16[1024,1536]{1,0:T(8,128)(2,1)}, bf16[1024,1536]{1,0:T(8,128)(2,1)}, u32[]{:S(2)}, u32[]{:S(2)}) collective-permute-start(bf16[1024,1536]{1,0:T(8,128)(2,1)} %get-tuple-element.124), channel_id=1, source_target_pairs={{0,2},{2,0},{4,6},{6,4},{1,3},{3,1},{5,7},{7,5}} | collective-permute-start | bytes 9437192 | tf_op jit(solution)/shard_map/ppermute | solution.py:24
  1684.3 25.6 %collective-permute-start.40 = (f32[384,1152]{1,0:T(8,128)}, f32[384,1152]{1,0:T(8,128)}, u32[]{:S(2)}, u32[]{:S(2)}) collective-permute-start(f32[384,1152]{1,0:T(8,128)} %fusion.28), channel_id=1, source_target_pairs={{0,1},{1,0},{2,3},{3,2},{4,5},{5,4},{6,7},{7,6}} | collective-permute-start | bytes 5308424 | tf_op jit(solution)/shard_map/ppermute | solution.py:32
  (183 other events, 3659.9 us)
Sparse Core Ops, SparseCore 0:
  10.4 49.3 all-gather.15
  62.1 52.3 all-gather.13
  116.9 42.2 all-gather.11
  160.9 33.2 all-gather.17
  196.4 93.0 all-gather.19
  655.8 66.4 all-gather.25
  765.2 66.6 all-gather.27
  874.6 67.0 all-gather.29
  943.5 121.2 all-gather.23
  1068.2 365.9 reduce-scatter.1
  1436.9 17.7 all-gather.31
  1515.4 21.8 all-gather.21

commit v5 on v4

v5 whole, which is shorter than its diff:
```python
import functools

import jax
import jax.numpy as jnp
from jax import lax
from jax.experimental import pallas as pl
from jax.experimental.pallas import tpu as pltpu
from jax.sharding import PartitionSpec as P


HEAD_DIM = 64
EPS_NORM = 1e-6
F32 = jnp.float32
BF16 = jnp.bfloat16
LOG2E = 1.4426950408889634
VMEM_ALL = 60 * 1024 * 1024
SCALE = HEAD_DIM ** -0.5

SWAP_D = [(0, 1), (1, 0)]


SWAP_X = [(0, 1), (1, 0), (2, 3), (3, 2)]
SWAP_Y = [(0, 2), (2, 0), (1, 3), (3, 1)]


def pp_x(v):
    return lax.ppermute(v, 'model', SWAP_X)


def pp_y(v):
    return lax.ppermute(v, 'model', SWAP_Y)


def pp_d(v):
    return lax.ppermute(v, 'data', SWAP_D)


def rms_norm(values):
    return values * lax.rsqrt(jnp.mean(values * values, axis=-1, keepdims=True) + EPS_NORM)


def dot(a, b, dims):
    return lax.dot_general(a, b, (dims, ((), ())), preferred_element_type=F32)


def nn(a, b):
    return dot(a, b, ((1,), (0,)))


def nt(a, b):
    return dot(a, b, ((1,), (1,)))


def tn(a, b):
    return dot(a, b, ((0,), (0,)))


def pair_masks(rows):
    lane = lax.broadcasted_iota(jnp.int32, (rows, 128), 1)
    return lane < HEAD_DIM


CHUNK = 256


def masked_pair(q):
    low = pair_masks(CHUNK)
    zero = jnp.zeros_like(q)
    return jnp.concatenate([jnp.where(low, q, zero), jnp.where(low, zero, q)], axis=0)


def attn_fwd_body(*refs):
    q_ref, qn_ref, ko_ref, ks_ref, kno_ref, kns_ref, vo_ref, vs_ref = refs[:8]
    ctx_ref, lse_ref, a_ref, b_ref, ma_ref, mb_ref = refs[-6:]

    def scores(ko, ks, q, s_ref, m_ref):
        s = nt(jnp.concatenate([ko[...], ks[...]], axis=0), masked_pair(q))
        s_ref[...] = s
        m_ref[...] = jnp.max(s, axis=0, keepdims=True)

    def finish(s_ref, m_ref, i):
        rows = slice(i * CHUNK, (i + 1) * CHUNK)
        m = m_ref[...]
        p = jnp.exp2((s_ref[...] - m) * (SCALE * LOG2E))
        l = jnp.sum(p, axis=0, keepdims=True)
        pb = (p * (1.0 / l)).astype(BF16)
        lse = m * (SCALE * LOG2E) + jnp.log2(l)
        lse_ref[0, 0:1, rows] = lse[:, :CHUNK]
        lse_ref[0, 1:2, rows] = lse[:, CHUNK:]
        ctx_t = tn(jnp.concatenate([vo_ref[...], vs_ref[...]], axis=0), pb)
        ctx_t = jnp.concatenate([ctx_t[:HEAD_DIM, :CHUNK], ctx_t[HEAD_DIM:, CHUNK:]], axis=0)
        ctx_ref[0, rows, :] = ctx_t.T.astype(BF16)

    @pl.when(pl.program_id(0) == 0)
    def _():
        scores(ko_ref, ks_ref, q_ref[:CHUNK, :], a_ref, ma_ref)

    scores(ko_ref, ks_ref, q_ref[CHUNK:, :], b_ref, mb_ref)
    finish(a_ref, ma_ref, 0)
    scores(kno_ref, kns_ref, qn_ref[:CHUNK, :], a_ref, ma_ref)
    finish(b_ref, mb_ref, 1)


def attn_fwd(q, kv, kv_s, layer, layers, hist):
    tq, width = q.shape
    tk = kv.shape[0]
    pairs = width // 128
    last = pairs - 1

    def col(off):
        return lambda j: (0, j + off)

    def nxt(j):
        return (0, jnp.minimum(j + 1, last))

    extra = [] if hist is None else [hist]
    flops = 2 * 2 * tq * (2 * tk) * 256 * (width // HEAD_DIM)
    return pl.pallas_call(
        attn_fwd_body,
        grid=(pairs,),
        in_specs=[pl.BlockSpec((tq, 128), col(0)), pl.BlockSpec((tq, 128), nxt),
                  pl.BlockSpec((tk, 128), col(0)), pl.BlockSpec((tk, 128), col(0)),
                  pl.BlockSpec((tk, 128), nxt), pl.BlockSpec((tk, 128), nxt),
                  pl.BlockSpec((tk, 128), col(pairs)), pl.BlockSpec((tk, 128), col(pairs))]
        + [pl.BlockSpec(memory_space=pl.ANY)] * len(extra),
        out_specs=[pl.BlockSpec((1, tq, 128), lambda j: (layer, 0, j)),
                   pl.BlockSpec((1, 2, tq), lambda j: (j, 0, 0))],
        out_shape=[jax.ShapeDtypeStruct((layers, tq, width), BF16),
                   jax.ShapeDtypeStruct((pairs, 2, tq), F32)],
        input_output_aliases={8: 0} if extra else {},
        scratch_shapes=[pltpu.VMEM((2 * tk, 2 * CHUNK), F32), pltpu.VMEM((2 * tk, 2 * CHUNK), F32),
                        pltpu.VMEM((1, 2 * CHUNK), F32), pltpu.VMEM((1, 2 * CHUNK), F32)],
        compiler_params=pltpu.CompilerParams(dimension_semantics=('arbitrary',),
                                             vmem_limit_bytes=VMEM_ALL),
        cost_estimate=pl.CostEstimate(flops=flops, bytes_accessed=2 * (tq * width * 2 + 4 * tk * width),
                                      transcendentals=tq * 2 * tk * (width // HEAD_DIM)),
        name='attn_fwd',
    )(q, q, kv, kv_s, kv, kv_s, kv, kv_s, *extra)


def attn_bwd_body(*refs):
    q_ref, ko_ref, ks_ref, vo_ref, vs_ref, do_ref, lse_ref = refs[:7]
    dq_ref, dko_ref, dks_ref, dvo_ref, dvs_ref = refs[-5:]
    tk = ko_ref.shape[0]
    k = jnp.concatenate([ko_ref[...], ks_ref[...]], axis=0)
    v = jnp.concatenate([vo_ref[...], vs_ref[...]], axis=0)
    tq = q_ref.shape[0]
    chunk = 256
    low = pair_masks(chunk)
    for i in range(tq // chunk):
        rows = slice(i * chunk, (i + 1) * chunk)
        q = q_ref[rows, :]
        do = do_ref[rows, :]
        dqs = []
        for h in range(2):
            sel = low if h == 0 else ~low
            qm = jnp.where(sel, q, jnp.zeros_like(q))
            dom = jnp.where(sel, do, jnp.zeros_like(do))
            s = nt(k, qm)
            p = jnp.exp2(s * (SCALE * LOG2E) - lse_ref[0, h:h + 1, rows])
            dp = nt(v, dom).astype(BF16).astype(F32)
            delta = jnp.sum(p * dp, axis=0, keepdims=True)
            ds = (p * (dp - delta)).astype(BF16)
            dv = nn(p.astype(BF16), dom)
            dk = nn(ds, qm) * SCALE
            if i == 0 and h == 0:
                dvo_ref[...] = dv[:tk]
                dvs_ref[...] = dv[tk:]
                dko_ref[...] = dk[:tk]
                dks_ref[...] = dk[tk:]
            else:
                dvo_ref[...] += dv[:tk]
                dvs_ref[...] += dv[tk:]
                dko_ref[...] += dk[:tk]
                dks_ref[...] += dk[tk:]
            dqs.append(tn(k, ds)[h * HEAD_DIM:(h + 1) * HEAD_DIM, :] * SCALE)
        dq_ref[0, rows, :] = jnp.concatenate(dqs, axis=0).T.astype(BF16)


def attn_bwd(q, kv, kv_s, d_ctx, lse, layer, layers, hist):
    tq, width = q.shape
    tk = kv.shape[0]
    pairs = width // 128

    def col(off):
        return lambda j: (0, j + off)

    flops = 5 * 2 * tq * (2 * tk) * 256 * (width // HEAD_DIM)
    kblk = pl.BlockSpec((tk, 128), col(0))
    extra = [] if hist is None else [hist]
    return pl.pallas_call(
        attn_bwd_body,
        grid=(pairs,),
        in_specs=[pl.BlockSpec((tq, 128), col(0)),
                  kblk, kblk,
                  pl.BlockSpec((tk, 128), col(pairs)), pl.BlockSpec((tk, 128), col(pairs)),
                  pl.BlockSpec((tq, 128), col(0)),
                  pl.BlockSpec((1, 2, tq), lambda j: (j, 0, 0))]
        + [pl.BlockSpec(memory_space=pl.ANY)] * len(extra),
        out_specs=[pl.BlockSpec((1, tq, 128), lambda j: (layer, 0, j)), kblk, kblk, kblk, kblk],
        out_shape=[jax.ShapeDtypeStruct((layers, tq, width), BF16)]
        + [jax.ShapeDtypeStruct((tk, width), F32)] * 4,
        input_output_aliases={7: 0} if extra else {},
        compiler_params=pltpu.CompilerParams(dimension_semantics=('arbitrary',),
                                             vmem_limit_bytes=VMEM_ALL),
        cost_estimate=pl.CostEstimate(flops=flops, bytes_accessed=2 * (2 * tq * width * 2 + 4 * tk * width) + 16 * tk * width,
                                      transcendentals=tq * 2 * tk * (width // HEAD_DIM)),
        name='attn_bwd',
    )(q, kv, kv_s, kv, kv_s, d_ctx, lse, *extra)


GELU_C = 0.7978845608028654
GELU_A = 0.044715
BLOCK_F = 768
SUB_F = 768
ROWS = (slice(0, 256), slice(256, 512))


def mlp_fwd_body(*refs):
    h_ref, w1_ref, w2_ref = refs[:3]
    z_ref, g_ref, x_ref, m_ref, acc_ref = refs[-5:]
    j = pl.program_id(0)

    @pl.when(j == 0)
    def _():
        hf = h_ref[...].astype(F32)
        acc_ref[...] = hf
        m_ref[0] = (hf * lax.rsqrt(jnp.mean(hf * hf, axis=-1, keepdims=True) + EPS_NORM)).astype(BF16)

    for rows in ROWS:
        z = nt(m_ref[0, rows, :], w1_ref[...]).astype(BF16)
        z_ref[rows, :] = z
        zf = z.astype(F32)
        t = jnp.tanh(zf * (GELU_C + (GELU_A * GELU_C) * (zf * zf)))
        half = 0.5 * zf
        g_ref[0, rows, :] = (half + half * t).astype(BF16)
    for rows in ROWS:
        acc_ref[rows, :] += nn(g_ref[0, rows, :], w2_ref[...])

    @pl.when(j == pl.num_programs(0) - 1)
    def _():
        x_ref[...] = acc_ref[...].astype(BF16)


def mlp_fwd(h, w1t, w2, layer, layers, hist):
    t, dim = h.shape
    hidden = w2.shape[0]
    whole = pl.BlockSpec((t, dim), lambda j: (0, 0))
    wblk = pl.BlockSpec((BLOCK_F, dim), lambda j: (j, 0))
    extra = [] if hist is None else [hist]
    return pl.pallas_call(
        mlp_fwd_body,
        grid=(hidden // BLOCK_F,),
        in_specs=[whole, wblk, wblk] + [pl.BlockSpec(memory_space=pl.ANY)] * len(extra),
        out_specs=[pl.BlockSpec((t, BLOCK_F), lambda j: (0, j)),
                   pl.BlockSpec((1, t, BLOCK_F), lambda j: (j, 0, 0)), whole,
                   pl.BlockSpec((1, t, dim), lambda j: (layer, 0, 0))],
        out_shape=[jax.ShapeDtypeStruct((t, hidden), BF16),
                   jax.ShapeDtypeStruct((hidden // BLOCK_F, t, BLOCK_F), BF16),
                   jax.ShapeDtypeStruct((t, dim), BF16),
                   jax.ShapeDtypeStruct((layers, t, dim), BF16)],
        scratch_shapes=[pltpu.VMEM((t, dim), F32)],
        input_output_aliases={3: 3} if extra else {},
        compiler_params=pltpu.CompilerParams(dimension_semantics=('arbitrary',), vmem_limit_bytes=VMEM_ALL),
        cost_estimate=pl.CostEstimate(flops=4 * t * dim * hidden, bytes_accessed=4 * dim * hidden + 4 * t * hidden,
                                      transcendentals=t * hidden),
        name='mlp_fwd',
    )(h, w1t, w2, *extra)


def mlp_bwd_body(*refs):
    d_ref, h_ref, z_ref, w1_ref, w2_ref = refs[:5]
    up_ref, mid_ref, acc_ref = refs[-3:]
    j = pl.program_id(0)

    @pl.when(j == 0)
    def _():
        acc_ref[...] = jnp.zeros_like(acc_ref)

    for i in range(0, BLOCK_F, SUB_F):
        cols = slice(i, i + SUB_F)
        for rows in ROWS:
            da = nt(d_ref[rows, :], w2_ref[cols, :]).astype(BF16).astype(F32)
            zf = z_ref[rows, cols].astype(F32)
            z2 = zf * zf
            t = jnp.tanh(zf * (GELU_C + (GELU_A * GELU_C) * z2))
            slope = (1.0 + t) * (0.5 + (1.0 - t) * (zf * (0.5 * GELU_C + (1.5 * GELU_A * GELU_C) * z2)))
            up_ref[0, rows, cols] = (da * slope).astype(BF16)
    for rows in ROWS:
        acc_ref[rows, :] += nn(up_ref[0, rows, :], w1_ref[...])

    @pl.when(j == pl.num_programs(0) - 1)
    def _():
        dn = acc_ref[...].astype(BF16).astype(F32)
        hf = h_ref[...].astype(F32)
        inv = lax.rsqrt(jnp.mean(hf * hf, axis=-1, keepdims=True) + EPS_NORM)
        proj = jnp.mean(hf * dn, axis=-1, keepdims=True)
        mid_ref[0] = (d_ref[...].astype(F32) + inv * dn - hf * (inv * inv * inv * proj)).astype(BF16)


def mlp_bwd(d_next, h, z, w1t, w2, layer, layers, hist, mid_hist):
    t, dim = h.shape
    hidden = w2.shape[0]
    whole = pl.BlockSpec((t, dim), lambda j: (0, 0))
    wblk = pl.BlockSpec((BLOCK_F, dim), lambda j: (j, 0))
    hspec = pl.BlockSpec((1, t, BLOCK_F), lambda j: (layer, 0, j))
    extra = [] if hist is None else [hist, mid_hist]
    return pl.pallas_call(
        mlp_bwd_body,
        grid=(hidden // BLOCK_F,),
        in_specs=[whole, whole, pl.BlockSpec((t, BLOCK_F), lambda j: (0, j)), wblk, wblk]
        + [pl.BlockSpec(memory_space=pl.ANY)] * len(extra),
        out_specs=[hspec, pl.BlockSpec((1, t, dim), lambda j: (layer, 0, 0))],
        out_shape=[jax.ShapeDtypeStruct((layers, t, hidden), BF16), jax.ShapeDtypeStruct((layers, t, dim), BF16)],
        scratch_shapes=[pltpu.VMEM((t, dim), F32)],
        input_output_aliases={5: 0, 6: 1} if extra else {},
        compiler_params=pltpu.CompilerParams(dimension_semantics=('arbitrary',), vmem_limit_bytes=VMEM_ALL),
        cost_estimate=pl.CostEstimate(flops=4 * t * dim * hidden, bytes_accessed=4 * dim * hidden + 4 * t * hidden,
                                      transcendentals=t * hidden),
        name='mlp_bwd',
    )(d_next, h, z, w1t, w2, *extra)


def join_body(count, core_ref, *refs):
    for n in range(count):
        own, other, out = refs[n], refs[count + n], refs[2 * count + n]
        for i, src in enumerate((own, other)):
            @pl.when(pl.program_id(0) == i)
            def _():
                out[...] = src[...]


def join_call(core, body, grid, own, other, in_specs, out_specs, out_shape):
    size = sum(v.size for v in own)
    return pl.pallas_call(
        body,
        grid_spec=pltpu.PrefetchScalarGridSpec(num_scalar_prefetch=1, grid=grid, in_specs=in_specs * 2, out_specs=out_specs),
        out_shape=out_shape,
        compiler_params=pltpu.CompilerParams(dimension_semantics=('arbitrary', 'arbitrary'), vmem_limit_bytes=VMEM_ALL),
        cost_estimate=pl.CostEstimate(flops=8 * size, bytes_accessed=16 * size, transcendentals=0),
    )(core.reshape(1), *own, *other)


def join(core, own, other, axes, parts):
    in_specs, out_specs, out_shape = [], [], []
    for v, axis in zip(own, axes):
        rows, cols = v.shape[0], v.shape[1] // parts
        in_specs.append(pl.BlockSpec((rows, cols), lambda i, j, c: (0, j)))
        if axis == 0:
            out_shape.append(jax.ShapeDtypeStruct((2 * rows, v.shape[1]), v.dtype))
            out_specs.append(pl.BlockSpec((rows, cols), lambda i, j, c: ((c[0] + i) % 2, j)))
        else:
            out_shape.append(jax.ShapeDtypeStruct((rows, 2 * v.shape[1]), v.dtype))
            out_specs.append(pl.BlockSpec((rows, cols), lambda i, j, c, parts=parts: (0, ((c[0] + i) % 2) * parts + j)))
    return join_call(core, functools.partial(join_body, len(own)), (2, parts), own, other, in_specs, out_specs, out_shape)


def join_flip_body(core_ref, oa_ref, ob_ref, sa_ref, sb_ref, out_ref):
    for i, srcs in enumerate(((oa_ref, ob_ref), (sa_ref, sb_ref))):
        for j, src in enumerate(srcs):
            @pl.when((pl.program_id(0) == i) & (pl.program_id(1) == j))
            def _():
                out_ref[...] = src[...].T


def join_flip(core, own, other):
    rows, cols = own[0].shape
    block = pl.BlockSpec((rows, cols), lambda i, j, c: (0, 0))
    return join_call(core, join_flip_body, (2, 2), own, other, [block] * 2,
                     pl.BlockSpec((cols, rows), lambda i, j, c: (j, (c[0] + i) % 2)),
                     jax.ShapeDtypeStruct((2 * cols, 2 * rows), F32))


def gather_pieces(part_a, part_b):
    xa, xb = pp_x(part_a), pp_x(part_b)
    ya, yb = pp_y(part_a), pp_y(part_b)
    da, db = pp_y(xa), pp_x(yb)
    own = [(xa, xb), (ya, yb), (da, db)]
    return own, [(pp_d(a), pp_d(b)) for a, b in own]


def own_terms(tile, first, second):
    order = (3, first, second, 0)
    sent = {r: pp_d(tile(r, 1)) for r in order}
    return {r: tile(r, 0) + sent[r] for r in order}


def reduce_terms(total, pp_first, pp_second, first, second):
    here = total[0] + pp_first(total[first])
    there = total[second] + pp_first(total[3])
    return here + pp_second(there)


BOTH = ('model', 'data')


def solution(mesh):
    spec_col = P(None, 'model')
    spec_row = P('model', None)
    spec_act = P('data', None, None)
    spec_rep = P(None, None)

    def device_step(x_in, cot_out, step_emb, w_q, w_k, w_v, w_o, w_1, w_2):
        layer_count, dim = step_emb.shape
        core = lax.axis_index('data')
        chip = lax.axis_index('model')
        chip_x = lax.rem(chip, 2)
        chip_y = lax.div(chip, 2)
        nbr_x = chip + 1 - 2 * chip_x
        nbr_y = lax.rem(chip + 2, 4)
        diag = lax.rem(nbr_x + 2, 4)
        chips = (chip, nbr_x, nbr_y, diag)
        hid = w_q.shape[1]
        half_d = dim // 2

        def take(v, which, axis, size):
            return lax.dynamic_slice_in_dim(v, which * size, size, axis)

        def put(buf, v, which, axis):
            return lax.dynamic_update_slice_in_dim(buf, v, which * v.shape[axis], axis)

        def gather(v):
            return lax.all_gather(v, BOTH, axis=0, tiled=True)

        def scatter(v):
            return lax.psum_scatter(v, BOTH, scatter_dimension=0, tiled=True)

        def after(v, *deps):
            return lax.optimization_barrier((v,) + deps)[0]

        def keep(hist, v, layer):
            if hist is None:
                hist = jnp.zeros((layer_count,) + v.shape, v.dtype)
            return lax.dynamic_update_slice(hist, v[None], (layer, 0, 0))

        def my_tokens(v):
            mine = lax.dynamic_index_in_dim(v, chip_x, 0, keepdims=False)
            half = mine.shape[0] // 2
            recv = pp_d(take(mine, 1 - core, 0, half))
            return jnp.where(core == chip_y, take(mine, core, 0, half), recv)

        def gather_permuted(local):
            own = take(local, core, 0, local.shape[0] // 2)
            rows = own.shape[0] // 2
            p_own, p_sib = gather_pieces(own[:rows], own[rows:])
            full = put(jnp.zeros((4 * local.shape[0], dim), BF16), local, chip, 0)
            for r in (1, 2, 3):
                for part in (0, 1):
                    full = put(full, p_own[r - 1][part], 4 * chips[r] + 2 * core + part, 0)
                    full = put(full, p_sib[r - 1][part], 4 * chips[r] + 2 * (1 - core) + part, 0)
            return full

        x_cur = my_tokens(x_in)
        qkv_t = jnp.concatenate([w_q, w_k, w_v], axis=1).T
        qkv_all = gather(take(qkv_t, core, 0, qkv_t.shape[0] // 2))
        o_all = gather(take(w_o, core, 0, hid // 2))
        w2 = gather_permuted(w_2)
        w1 = gather_permuted(w_1.T)
        wq, wk, wv = [jnp.concatenate([take(qkv_all, 3 * c + i, 0, hid) for c in chips], axis=0) for i in range(3)]
        wo = jnp.concatenate([take(o_all, c, 0, hid) for c in chips], axis=0)
        d_cur = my_tokens(cot_out)

        saved = []
        g_mine = []
        u_hist = m_hist = ctx_hist = None
        for layer in range(layer_count):
            s = x_cur.astype(F32) + step_emb[layer].astype(F32)
            u = rms_norm(s).astype(BF16)
            kv = jnp.concatenate([nt(u, wk).astype(BF16), nt(u, wv).astype(BF16)], axis=1)
            kv_s = pp_d(kv)
            q = nt(u, wq).astype(BF16)
            ctx_hist, lse = attn_fwd(q, kv, kv_s, layer, layer_count, ctx_hist)
            h = (s + nn(ctx_hist[layer], wo)).astype(BF16)
            z, g, x_next, m_hist = mlp_fwd(h, w1, w2, layer, layer_count, m_hist)
            g_mine.append(lax.all_to_all(g.reshape(-1, g.shape[-1]), BOTH, split_axis=0, concat_axis=0, tiled=True))
            u_hist = keep(u_hist, u, layer)
            u_hist, x_next = lax.optimization_barrier((u_hist, x_next))
            saved.append((x_cur, q, kv, kv_s, lse, h, z))
            x_cur = x_next

        def flat(v):
            return v.reshape(-1, v.shape[-1])

        up_hist = mid_hist = dq_hist = dk_hist = dv_hist = None
        next_all = [None] * layer_count
        for layer in reversed(range(layer_count)):
            x_l, q, kv, kv_s, lse, h, z = saved[layer]
            d_next = d_cur
            next_all[layer] = gather(d_next)
            up_hist, mid_hist = mlp_bwd(d_next, h, z, w1, w2, layer, layer_count, up_hist, mid_hist)
            d_mid = mid_hist[layer]
            if layer == 0:
                up_f, m_f = flat(up_hist), flat(m_hist)
                term_1a, d_mid, up_f = lax.optimization_barrier((tn(up_f, m_f[:, :half_d]), d_mid, up_f))
                grad_1a = scatter(term_1a)
                term_1b = tn(up_f, m_f[:, half_d:])
                term_1b, d_mid = lax.optimization_barrier((term_1b, d_mid))
                grad_1b = scatter(term_1b)
            d_ctx = nt(d_mid, wo).astype(BF16)
            dq_hist, dko, dks, dvo, dvs = attn_bwd(q, kv, kv_s, d_ctx, lse, layer, layer_count, dq_hist)
            dk = (dko + pp_d(dks)).astype(BF16)
            dv = (dvo + pp_d(dvs)).astype(BF16)
            dk_hist, dv_hist = keep(dk_hist, dk, layer), keep(dv_hist, dv, layer)
            d_norm1 = (nn(dq_hist[layer], wq) + nn(dk, wk) + nn(dv, wv)).astype(BF16)
            s = x_l.astype(F32) + step_emb[layer].astype(F32)
            norm_pull_x = jax.vjp(rms_norm, s)[1]
            d_cur = (d_mid.astype(F32) + norm_pull_x(d_norm1.astype(F32))[0]).astype(BF16)
            if layer > 0:
                d_cur, dk_hist, dv_hist = lax.optimization_barrier((d_cur, dk_hist, dv_hist))

        mid_half = [lax.optimization_barrier(take(flat(mid_hist), w, 1, half_d)) for w in (core, 1 - core)]
        u_half = [lax.optimization_barrier(take(flat(u_hist), w, 1, half_d)) for w in (core, 1 - core)]

        def cols(v, r):
            return flat(v)[:, r * hid:(r + 1) * hid]

        t_o = own_terms(lambda r, half: tn(cols(ctx_hist, r), mid_half[half]), 2, 1)
        t_q = own_terms(lambda r, half: tn(u_half[half], cols(dq_hist, r)), 1, 2)
        t_k = own_terms(lambda r, half: tn(u_half[half], cols(dk_hist, r)), 1, 2)
        t_v = own_terms(lambda r, half: tn(u_half[half], cols(dv_hist, r)), 2, 1)
        own_o = reduce_terms(t_o, pp_y, pp_x, 2, 1)
        own_q = reduce_terms(t_q, pp_x, pp_y, 1, 2)
        own_k = reduce_terms(t_k, pp_x, pp_y, 1, 2)
        own_v = reduce_terms(t_v, pp_y, pp_x, 2, 1)

        def ordered(own, sib, axis):
            size = own.shape[axis]
            shape = own.shape[:axis] + (2 * size,) + own.shape[axis + 1:]
            return put(put(jnp.zeros(shape, own.dtype), own, core, axis), sib, 1 - core, axis)

        other_half = pp_d(d_cur)
        whole = ordered(d_cur, other_half, 0)
        to_row = [(2 * c + d, 2 * (c ^ 2) + d) for c in range(4) for d in range(2) if c // 2 == d]
        from_y = lax.ppermute(whole, BOTH, to_row)
        row_seq = jnp.where(chip_y == core, whole, from_y)
        from_x = pp_x(row_seq)
        d_x = jnp.zeros((2,) + whole.shape, BF16)
        d_x = put(put(d_x, row_seq[None], chip_x, 0), from_x[None], 1 - chip_x, 0)

        ready = tuple(t[r] for t in (t_o, t_q, t_k, t_v) for r in (1, 2, 3))
        grad_2 = None
        for layer in reversed(range(layer_count)):
            term = tn(after(g_mine[layer], *ready), next_all[layer])
            grad_2 = term if grad_2 is None else grad_2 + term

        (grad_2,) = join(core, [grad_2], [pp_d(grad_2)], (0,), 4)
        grad_1 = join_flip(core, [grad_1a, grad_1b], [pp_d(grad_1a), pp_d(grad_1b)])
        own = [own_q, own_k, own_v, own_o]
        gq, gk, gv, go = join(core, own, [pp_d(v) for v in own], (0, 0, 0, 1), 1)
        return gq, gk, gv, go, grad_1, grad_2, d_x

    return jax.shard_map(device_step, mesh=mesh,
                         in_specs=(spec_act, spec_act, spec_rep, spec_col, spec_col, spec_col, spec_row, spec_col, spec_row),
                         out_specs=(spec_col, spec_col, spec_col, spec_row, spec_col, spec_row, spec_act),
                         check_vma=False)
```

time: 1790 us -> 1870 us (1.045)
  waiting for transfers between devices: 605 us -> 644 us
  matrix products: 358 us -> 385 us
    ppermute x9 -> x12, waiting for transfers between devices: 122 us -> 237 us  [pp_y(): return lax.ppermute(v, 'model', SWAP_Y)]
    ppermute x10 -> x13, waiting for transfers between devices: 135 us -> 243 us  [pp_x(): return lax.ppermute(v, 'model', SWAP_X)]
    all_to_all x4, waiting for transfers between devices: 235 us -> 143 us  [device_step(): lax.all_to_all(g.reshape(-1, g.shape[-1]), BOTH, split_axis=0, concat_axi...]
    all_gather x9 -> x6, waiting for transfers between devices: 84.9 us -> 0.03 us  [gather(): return lax.all_gather(v, BOTH, axis=0, tiled=True)]
    pallas_call x0 -> x3, Pallas kernels: none -> 28.1 us  [join_call(): pl.pallas_call(body, grid_spec=pltpu.PrefetchScalarGridSpec(num_scalar_pr...]
    dot_general x69 -> x70, matrix products: 358 us -> 385 us  [dot(): return lax.dot_general(a, b, (dims, ((), ())), preferred_element_type=F32)]
    pallas_call x4, Pallas kernels: 196 us -> 173 us  [attn_bwd(): pl.pallas_call(attn_bwd_body, grid=(pairs,), in_specs=[pl.BlockSpec((tq,...]
    dynamic_update_slice x17 -> x28, local copies, waits for them, and re-layouts: 36.6 us -> 54.7 us  [put(): return lax.dynamic_update_slice_in_dim(buf, v, which * v.shape[axis], axis)]
  transfers between devices with their start and end apart: 77 -> 88, of which waited for: 24 -> 23; matrix products, arithmetic and copies ran while one was open for 27% -> 30% of each run, Pallas kernels for 14% -> 26%
where the time goes in v5:
time: 1870 us; the launch traced here: 1860 us
  waiting for transfers between devices  644 us (34%)
  Pallas kernels  538 us (29%)
  matrix products  385 us (21%)
  local copies, waits for them, and re-layouts  149 us (8%)
  other arithmetic  65.1 us (3%)
  starting transfers between devices  63.5 us (3%)
    dot_general x70, matrix products, dot(): return lax.dot_general(a, b, (dims, ((), ())), preferred_element_type=F32)  385 us
    ppermute x13, waiting for transfers between devices, pp_x(): return lax.ppermute(v, 'model', SWAP_X)  243 us
    ppermute x12, waiting for transfers between devices, pp_y(): return lax.ppermute(v, 'model', SWAP_Y)  237 us
    pallas_call x4, Pallas kernels, attn_bwd(): pl.pallas_call(attn_bwd_body, grid=(pairs,), in_specs=[pl.BlockSpec((tq,...  173 us
    all_to_all x4, waiting for transfers between devices, device_step(): lax.all_to_all(g.reshape(-1, g.shape[-1]), BOTH, split_axis=0, concat_axi...  143 us
    pallas_call x4, Pallas kernels, mlp_bwd(): pl.pallas_call(mlp_bwd_body, grid=(hidden // BLOCK_F,), in_specs=[whole,...  126 us
    pallas_call x4, Pallas kernels, mlp_fwd(): pl.pallas_call(mlp_fwd_body, grid=(hidden // BLOCK_F,), in_specs=[whole,...  116 us
    pallas_call x4, Pallas kernels, attn_fwd(): pl.pallas_call(attn_fwd_body, grid=(pairs,), in_specs=[pl.BlockSpec((tq,...  94.3 us
  transfers between devices with their start and end apart: 88, of which 23 were waited for; matrix products, arithmetic and copies ran while one was open for 30% of the time, Pallas kernels for 26%

profile of v5, /device:TPU:0, one launch (start us, length us, event | category | flops | bytes accessed | tf_op | source)
XLA Modules:
  0.0 1860.5 jit_solution(16254903590108544237)
XLA Ops:
  16.2 6.6 copy.36
  40.4 7.4 broadcast.112.clone
  50.5 6.6 broadcast.112.clone.1
  59.5 17.1 collective-permute-done.2
  80.1 86.5 %collective-permute-done.14 = bf16[384,1536]{1,0:T(8,128)(2,1)} collective-permute-done((bf16[384,1536]{1,0:T(8,128)(2,1)}, bf16[384,1536]{1,0:T(8,128)(2,1)}, u32[]{:S(2)}, u32[]{:S(2)}) %collective-permute-start.14) | collective-permute-done | bytes 1179680 | tf_op jit(solution)/shard_map/ppermute | solution.py:27
  182.1 28.0 %collective-permute-done.16 = bf16[384,1536]{1,0:T(8,128)(2,1)S(1)} collective-permute-done((bf16[384,1536]{1,0:T(8,128)(2,1)S(1)}, bf16[384,1536]{1,0:T(8,128)(2,1)S(1)}, u32[]{:S(2)}, u32[]{:S(2)}) %collective-permute-start.16) | collective-permute-done | bytes 1179680 | tf_op jit(solution)/shard_map/ppermute | solution.py:27
  220.2 13.4 collective-permute-done.8
  236.3 22.7 %collective-permute-done.20 = bf16[384,1536]{1,0:T(8,128)(2,1)} collective-permute-done((bf16[384,1536]{1,0:T(8,128)(2,1)S(1)}, bf16[384,1536]{1,0:T(8,128)(2,1)}, u32[]{:S(2)}, u32[]{:S(2)}) %collective-permute-start.20) | collective-permute-done | bytes 1179680 | tf_op jit(solution)/shard_map/ppermute | solution.py:31
  269.4 14.8 collective-permute-done.10
  287.8 21.1 %collective-permute-done.22 = bf16[384,1536]{1,0:T(8,128)(2,1)} collective-permute-done((bf16[384,1536]{1,0:T(8,128)(2,1)}, bf16[384,1536]{1,0:T(8,128)(2,1)}, u32[]{:S(2)}, u32[]{:S(2)}) %collective-permute-start.22) | collective-permute-done | bytes 1179680 | tf_op jit(solution)/shard_map/ppermute | solution.py:31
  312.5 7.9 constant_dynamic-slice_fusion.17
  354.0 23.4 %attn_fwd.4 = (bf16[4,512,1536]{2,1,0:T(8,128)(2,1)}, f32[12,2,512]{2,1,0:T(2,128)}) custom-call(bf16[512,1536]{1,0:T(8,128)(2,1)} %convolution_convert_fusion.15.refs_0_.refs_1_, bf16[512,1536]{1,0:T(8,128)(2,1)} %convolution_convert_fusion.15.refs_0_.refs_1_, bf16[512,3072]{1,0:T(8,128)(2,1)} %pad_maximum_fusion.4.refs_2_.refs_4_.refs_6_.refs_1_.refs_3_, ...), custom_call_target="tpu_custom_call" | custom-call | flops 12884901888 | bytes 9437184 | tf_op jit(solution)/shard_map/attn_fwd/pallas_call | solution.py:118
  377.4 5.7 fusion.16.refs_0_.refs_1_
  383.1 29.3 %mlp_fwd.4 = (bf16[512,6144]{1,0:T(8,128)(2,1)}, bf16[8,512,768]{2,1,0:T(8,128)(2,1)}, bf16[512,1536]{1,0:T(8,128)(2,1)}, bf16[4,512,1536]{2,1,0:T(8,128)(2,1)}) custom-call(bf16[512,1536]{1,0:T(8,128)(2,1)} %fusion.16.refs_0_.refs_1_, bf16[6144,1536]{1,0:T(8,128)(2,1)} %constant_dynamic-update-slice_fusion.15.refs_1_.refs_3_, ...), custom_call_target="tpu_custom_call" | custom-call | flops 19327352832 | bytes 50331648 | tf_op jit(solution)/shard_map/mlp_fwd/pallas_call | solution.py:251
  414.9 5.2 convolution_convert_fusion.11
  433.5 23.5 %attn_fwd.5 = (bf16[4,512,1536]{2,1,0:T(8,128)(2,1)}, f32[12,2,512]{2,1,0:T(2,128)}) custom-call(bf16[512,1536]{1,0:T(8,128)(2,1)} %convolution_convert_fusion.12.refs_0_.refs_1_, bf16[512,1536]{1,0:T(8,128)(2,1)} %convolution_convert_fusion.12.refs_0_.refs_1_, bf16[512,3072]{1,0:T(8,128)(2,1)} %copy-done.26, ...), custom_call_target="tpu_custom_call", output_to_operand_aliasing={{0}: (8, {})} | custom-call | flops 12884901888 | bytes 9437184 | tf_op jit(solution)/shard_map/attn_fwd/pallas_call | solution.py:118
  457.0 5.7 fusion.17.refs_0_.refs_1_
  462.7 28.8 %mlp_fwd.5 = (bf16[512,6144]{1,0:T(8,128)(2,1)}, bf16[8,512,768]{2,1,0:T(8,128)(2,1)}, bf16[512,1536]{1,0:T(8,128)(2,1)}, bf16[4,512,1536]{2,1,0:T(8,128)(2,1)}) custom-call(bf16[512,1536]{1,0:T(8,128)(2,1)} %fusion.17.refs_0_.refs_1_, bf16[6144,1536]{1,0:T(8,128)(2,1)} %constant_dynamic-update-slice_fusion.15.refs_1_.refs_3_, ...), custom_call_target="tpu_custom_call", output_to_operand_aliasing={{3}: (3, {})} | custom-call | flops 19327352832 | bytes 50331648 | tf_op jit(solution)/shard_map/mlp_fwd/pallas_call | solution.py:251
  494.1 5.6 convolution_convert_fusion.8
  510.4 5.4 convolution_convert_fusion.9.refs_0_.refs_1_
  515.9 23.7 %attn_fwd.6 = (bf16[4,512,1536]{2,1,0:T(8,128)(2,1)}, f32[12,2,512]{2,1,0:T(2,128)}) custom-call(bf16[512,1536]{1,0:T(8,128)(2,1)} %convolution_convert_fusion.9.refs_0_.refs_1_, bf16[512,1536]{1,0:T(8,128)(2,1)} %convolution_convert_fusion.9.refs_0_.refs_1_, ...), custom_call_target="tpu_custom_call", output_to_operand_aliasing={{0}: (8, {})} | custom-call | flops 12884901888 | bytes 9437184 | tf_op jit(solution)/shard_map/attn_fwd/pallas_call | solution.py:118
  539.6 5.7 fusion.18.refs_0_.refs_1_
  545.3 29.1 %mlp_fwd.6 = (bf16[512,6144]{1,0:T(8,128)(2,1)}, bf16[8,512,768]{2,1,0:T(8,128)(2,1)}, bf16[512,1536]{1,0:T(8,128)(2,1)}, bf16[4,512,1536]{2,1,0:T(8,128)(2,1)}) custom-call(bf16[512,1536]{1,0:T(8,128)(2,1)} %fusion.18.refs_0_.refs_1_, bf16[6144,1536]{1,0:T(8,128)(2,1)} %constant_dynamic-update-slice_fusion.15.refs_1_.refs_3_, ...), custom_call_target="tpu_custom_call", output_to_operand_aliasing={{3}: (3, {})} | custom-call | flops 19327352832 | bytes 50331648 | tf_op jit(solution)/shard_map/mlp_fwd/pallas_call | solution.py:251
  576.9 5.2 convolution_convert_fusion.5
  592.1 23.8 %attn_fwd.7 = (bf16[4,512,1536]{2,1,0:T(8,128)(2,1)}, f32[12,2,512]{2,1,0:T(2,128)}) custom-call(bf16[512,1536]{1,0:T(8,128)(2,1)} %convolution_convert_fusion.6.refs_0_.refs_1_, bf16[512,1536]{1,0:T(8,128)(2,1)} %convolution_convert_fusion.6.refs_0_.refs_1_, bf16[512,3072]{1,0:T(8,128)(2,1)} %copy-done.27, ...), custom_call_target="tpu_custom_call", output_to_operand_aliasing={{0}: (8, {})} | custom-call | flops 12884901888 | bytes 9437184 | tf_op jit(solution)/shard_map/attn_fwd/pallas_call | solution.py:118
  615.9 5.6 fusion.19.refs_0_.refs_1_
  621.5 28.8 %mlp_fwd.7 = (bf16[512,6144]{1,0:T(8,128)(2,1)}, bf16[8,512,768]{2,1,0:T(8,128)(2,1)}, bf16[512,1536]{1,0:T(8,128)(2,1)}, bf16[4,512,1536]{2,1,0:T(8,128)(2,1)}) custom-call(bf16[512,1536]{1,0:T(8,128)(2,1)} %fusion.19.refs_0_.refs_1_, bf16[6144,1536]{1,0:T(8,128)(2,1)} %constant_dynamic-update-slice_fusion.15.refs_1_.refs_3_, ...), custom_call_target="tpu_custom_call", output_to_operand_aliasing={{3}: (3, {})} | custom-call | flops 19327352832 | bytes 50331648 | tf_op jit(solution)/shard_map/mlp_fwd/pallas_call | solution.py:251
  650.3 31.2 %mlp_bwd.4 = (bf16[4,512,6144]{2,1,0:T(8,128)(2,1)}, bf16[4,512,1536]{2,1,0:T(8,128)(2,1)}) custom-call(bf16[512,1536]{1,0:T(8,128)(2,1)} %bitcast_select_fusion.refs_0_, bf16[512,1536]{1,0:T(8,128)(2,1)} %fusion.19.refs_0_.refs_1_, bf16[512,6144]{1,0:T(8,128)(2,1)} %get-tuple-element.102.refs_2_, ...), custom_call_target="tpu_custom_call" | custom-call | flops 19327352832 | bytes 50331648 | tf_op jit(solution)/shard_map/mlp_bwd/pallas_call | solution.py:308
  681.5 5.9 convolution_convert_fusion.3.refs_5_
  687.4 43.3 %attn_bwd.4 = (bf16[4,512,1536]{2,1,0:T(8,128)(2,1)}, f32[512,1536]{1,0:T(8,128)}, f32[512,1536]{1,0:T(8,128)}, f32[512,1536]{1,0:T(8,128)}, f32[512,1536]{1,0:T(8,128)}) custom-call(bf16[512,1536]{1,0:T(8,128)(2,1)} %convolution_convert_fusion.6.refs_0_.refs_1_, bf16[512,3072]{1,0:T(8,128)(2,1)} %copy-done.27, ...), custom_call_target="tpu_custom_call" | custom-call | flops 32212254720 | bytes 25165824 | tf_op jit(solution)/shard_map/attn_bwd/pallas_call | solution.py:191
  731.4 5.5 collective-permute-done.31
  761.9 31.9 %mlp_bwd.5 = (bf16[4,512,6144]{2,1,0:T(8,128)(2,1)}, bf16[4,512,1536]{2,1,0:T(8,128)(2,1)}) custom-call(bf16[512,1536]{1,0:T(8,128)(2,1)} %fusion.5.refs_0_, bf16[512,1536]{1,0:T(8,128)(2,1)} %fusion.18.refs_0_.refs_1_, bf16[512,6144]{1,0:T(8,128)(2,1)} %get-tuple-element.111.refs_2_, ...), custom_call_target="tpu_custom_call", output_to_operand_aliasing={{0}: (5, {}), {1}: (6, {})} | custom-call | flops 19327352832 | bytes 50331648 | tf_op jit(solution)/shard_map/mlp_bwd/pallas_call | solution.py:308
  793.8 5.5 convolution_convert_fusion.2.refs_5_
  799.3 43.2 %attn_bwd.5 = (bf16[4,512,1536]{2,1,0:T(8,128)(2,1)}, f32[512,1536]{1,0:T(8,128)}, f32[512,1536]{1,0:T(8,128)}, f32[512,1536]{1,0:T(8,128)}, f32[512,1536]{1,0:T(8,128)}) custom-call(bf16[512,1536]{1,0:T(8,128)(2,1)} %convolution_convert_fusion.9.refs_0_.refs_1_, ...), custom_call_target="tpu_custom_call", output_to_operand_aliasing={{0}: (7, {})} | custom-call | flops 32212254720 | bytes 25165824 | tf_op jit(solution)/shard_map/attn_bwd/pallas_call | solution.py:191
  843.1 5.4 collective-permute-done.33
  870.2 32.0 %mlp_bwd.6 = (bf16[4,512,6144]{2,1,0:T(8,128)(2,1)}, bf16[4,512,1536]{2,1,0:T(8,128)(2,1)}) custom-call(bf16[512,1536]{1,0:T(8,128)(2,1)} %fusion.7.refs_0_, bf16[512,1536]{1,0:T(8,128)(2,1)} %fusion.17.refs_0_.refs_1_, bf16[512,6144]{1,0:T(8,128)(2,1)} %get-tuple-element.123.refs_2_, ...), custom_call_target="tpu_custom_call", output_to_operand_aliasing={{0}: (5, {}), {1}: (6, {})} | custom-call | flops 19327352832 | bytes 50331648 | tf_op jit(solution)/shard_map/mlp_bwd/pallas_call | solution.py:308
  902.2 5.5 convolution_convert_fusion.1.refs_5_
  907.7 43.1 %attn_bwd.6 = (bf16[4,512,1536]{2,1,0:T(8,128)(2,1)}, f32[512,1536]{1,0:T(8,128)}, f32[512,1536]{1,0:T(8,128)}, f32[512,1536]{1,0:T(8,128)}, f32[512,1536]{1,0:T(8,128)}) custom-call(bf16[512,1536]{1,0:T(8,128)(2,1)} %convolution_convert_fusion.12.refs_0_.refs_1_, bf16[512,3072]{1,0:T(8,128)(2,1)} %copy-done.26, ...), custom_call_target="tpu_custom_call", output_to_operand_aliasing={{0}: (7, {})} | custom-call | flops 32212254720 | bytes 25165824 | tf_op jit(solution)/shard_map/attn_bwd/pallas_call | solution.py:191
  951.4 5.4 collective-permute-done.35
  978.6 31.4 %mlp_bwd.7 = (bf16[4,512,6144]{2,1,0:T(8,128)(2,1)}, bf16[4,512,1536]{2,1,0:T(8,128)(2,1)}) custom-call(bf16[512,1536]{1,0:T(8,128)(2,1)} %fusion.9.refs_0_, bf16[512,1536]{1,0:T(8,128)(2,1)} %fusion.16.refs_0_.refs_1_, bf16[512,6144]{1,0:T(8,128)(2,1)} %get-tuple-element.135.refs_2_, ...), custom_call_target="tpu_custom_call", output_to_operand_aliasing={{0}: (5, {}), {1}: (6, {})} | custom-call | flops 19327352832 | bytes 50331648 | tf_op jit(solution)/shard_map/mlp_bwd/pallas_call | solution.py:308
  1012.6 26.6 %fusion.14 = f32[6144,768]{1,0:T(8,128)} fusion(bf16[2048,6144]{1,0:T(8,128)(2,1)} %bitcast.143, bf16[2048,1536]{1,0:T(8,128)(2,1)} %bitcast.185), kind=kOutput, calls=%fused_computation.47 | convolution fusion | flops 19327352832 | bytes 47185920 | tf_op jit(solution)/shard_map/dot_general | solution.py:43
  1039.2 26.7 %fusion.12 = f32[6144,768]{1,0:T(8,128)} fusion(bf16[2048,6144]{1,0:T(8,128)(2,1)} %bitcast.144, bf16[2048,1536]{1,0:T(8,128)(2,1)} %bitcast.186), kind=kOutput, calls=%fused_computation.45 | convolution fusion | flops 19327352832 | bytes 47185920 | tf_op jit(solution)/shard_map/dot_general | solution.py:43
  1072.0 6.7 convolution_convert_fusion.refs_5_
  1078.7 43.3 %attn_bwd.7 = (bf16[4,512,1536]{2,1,0:T(8,128)(2,1)}, f32[512,1536]{1,0:T(8,128)}, f32[512,1536]{1,0:T(8,128)}, f32[512,1536]{1,0:T(8,128)}, f32[512,1536]{1,0:T(8,128)}) custom-call(bf16[512,1536]{1,0:T(8,128)(2,1)} %convolution_convert_fusion.15.refs_0_.refs_1_, ...), custom_call_target="tpu_custom_call", output_to_operand_aliasing={{0}: (7, {})} | custom-call | flops 32212254720 | bytes 25165824 | tf_op jit(solution)/shard_map/attn_bwd/pallas_call | solution.py:191
  1122.3 8.1 constant_dynamic-slice_fusion.1
  1144.5 5.3 fusion.102
  1167.9 12.1 all-to-all-done.3
  1184.1 5.5 fusion.176
  1205.4 103.2 %collective-permute-done.64 = f32[384,768]{1,0:T(8,128)S(1)} collective-permute-done((f32[384,768]{1,0:T(8,128)S(1)}, f32[384,768]{1,0:T(8,128)S(1)}, u32[]{:S(2)}, u32[]{:S(2)}) %collective-permute-start.64) | collective-permute-done | bytes 1179680 | tf_op jit(solution)/shard_map/ppermute | solution.py:31
  1331.9 5.3 fusion.70
  1369.8 87.4 %all-to-all-done = bf16[8,512,768]{2,1,0:T(8,128)(2,1)} async-done(((bf16[8,512,768]{2,1,0:T(8,128)(2,1)}), bf16[8,512,768]{2,1,0:T(8,128)(2,1)}, u32[]{:S(2)}, u32[]{:S(2)}) %all-to-all-start) | async-done | bytes 6291488 | tf_op jit(solution)/shard_map/all_to_all | solution.py:475
  1495.1 16.4 fusion.196
  1511.5 43.2 %all-to-all-done.2 = bf16[8,512,768]{2,1,0:T(8,128)(2,1)} async-done(((bf16[8,512,768]{2,1,0:T(8,128)(2,1)}), bf16[8,512,768]{2,1,0:T(8,128)(2,1)}, u32[]{:S(2)}, u32[]{:S(2)}) %all-to-all-start.2) | async-done | bytes 6291488 | tf_op jit(solution)/shard_map/all_to_all | solution.py:475
  1557.4 46.7 %collective-permute-done.57 = f32[768,384]{1,0:T(8,128)} collective-permute-done((f32[768,384]{1,0:T(8,128)}, f32[768,384]{1,0:T(8,128)}, u32[]{:S(2)}, u32[]{:S(2)}) %collective-permute-start.57) | collective-permute-done | bytes 1179680 | tf_op jit(solution)/shard_map/ppermute | solution.py:31
  1609.5 16.3 fusion.197
  1625.8 16.3 fusion.198
  1642.6 20.4 %add_add_fusion.4.refs_0_ = f32[768,1536]{1,0:T(8,128)} fusion(f32[768,1536]{1,0:T(8,128)} %fusion.198, f32[768,1536]{1,0:T(8,128)} %fusion.196, f32[768,1536]{1,0:T(8,128)} %fusion.197, bf16[4096,768]{1,0:T(8,128)(2,1)} %bitcast.42, bf16[4096,1536]{1,0:T(8,128)(2,1)} %all-gather.17.cloned.1.call-done), kind=kOutput, calls=%fused_computation.9 | convolution fusion | flops 9667215360 | bytes 37748736 | tf_op jit(solution)/shard_map/dot_general | solution.py:43
  1675.8 15.2 collective-permute-done.54
  1695.5 22.7 %collective-permute-done.58 = f32[768,384]{1,0:T(8,128)} collective-permute-done((f32[768,384]{1,0:T(8,128)S(1)}, f32[768,384]{1,0:T(8,128)}, u32[]{:S(2)}, u32[]{:S(2)}) %collective-permute-start.58) | collective-permute-done | bytes 1179680 | tf_op jit(solution)/shard_map/ppermute | solution.py:27
  1725.4 84.7 %collective-permute-done.46 = f32[768,384]{1,0:T(8,128)} collective-permute-done((f32[768,384]{1,0:T(8,128)S(1)}, f32[768,384]{1,0:T(8,128)}, u32[]{:S(2)}, u32[]{:S(2)}) %collective-permute-start.46) | collective-permute-done | bytes 1179680 | tf_op jit(solution)/shard_map/ppermute | solution.py:27
  1810.6 6.2 fusion.137.refs_1_
  1820.1 7.8 shard_map.144
  1831.6 11.5 shard_map.146
  1844.5 8.8 shard_map.145
  (658 shorter events, 421.5 us)
Async XLA Ops:
  7.2 305.3 %all-gather.7.cloned.1.call-start = ((), (), s32[]{:S(2)}) async-start(), calls=%async_computation.6 | async-start | bytes 15925248 | tf_op jit(solution)/shard_map/all_gather | solution.py:423
  16.1 329.7 %all-gather.9.cloned.1.call-start = ((), (), s32[]{:S(2)}) async-start(), calls=%async_computation.7 | async-start | bytes 5308416 | tf_op jit(solution)/shard_map/all_gather | solution.py:423
  26.5 50.1 %collective-permute-start.2 = (bf16[384,1536]{1,0:T(8,128)(2,1)}, bf16[384,1536]{1,0:T(8,128)(2,1)}, u32[]{:S(2)}, u32[]{:S(2)}) collective-permute-start(bf16[384,1536]{1,0:T(8,128)(2,1)} %get-tuple-element.210), channel_id=1, source_target_pairs={{0,2},{2,0},{4,6},{6,4},{1,3},{3,1},{5,7},{7,5}} | collective-permute-start | bytes 3538952 | tf_op jit(solution)/shard_map/ppermute | solution.py:27
  29.9 151.3 %collective-permute-start.6 = (bf16[384,1536]{1,0:T(8,128)(2,1)}, bf16[384,1536]{1,0:T(8,128)(2,1)}, u32[]{:S(2)}, u32[]{:S(2)}) collective-permute-start(bf16[384,1536]{1,0:T(8,128)(2,1)} %get-tuple-element.210), channel_id=1, source_target_pairs={{0,4},{4,0},{2,6},{6,2},{1,5},{5,1},{3,7},{7,3}} | collective-permute-start | bytes 3538952 | tf_op jit(solution)/shard_map/ppermute | solution.py:31
  31.4 143.3 %collective-permute-start.4 = (bf16[384,1536]{1,0:T(8,128)(2,1)}, bf16[384,1536]{1,0:T(8,128)(2,1)}, u32[]{:S(2)}, u32[]{:S(2)}) collective-permute-start(bf16[384,1536]{1,0:T(8,128)(2,1)} %get-tuple-element.209), channel_id=1, source_target_pairs={{0,2},{2,0},{4,6},{6,4},{1,3},{3,1},{5,7},{7,5}} | collective-permute-start | bytes 3538952 | tf_op jit(solution)/shard_map/ppermute | solution.py:27
  35.1 131.5 %collective-permute-start.14 = (bf16[384,1536]{1,0:T(8,128)(2,1)}, bf16[384,1536]{1,0:T(8,128)(2,1)}, u32[]{:S(2)}, u32[]{:S(2)}) collective-permute-start(bf16[384,1536]{1,0:T(8,128)(2,1)} %get-tuple-element.204), channel_id=1, source_target_pairs={{0,2},{2,0},{4,6},{6,4},{1,3},{3,1},{5,7},{7,5}} | collective-permute-start | bytes 3538952 | tf_op jit(solution)/shard_map/ppermute | solution.py:27
  39.5 131.2 %collective-permute-start = (bf16[512,1536]{1,0:T(8,128)(2,1)}, bf16[512,1536]{1,0:T(8,128)(2,1)S(1)}, u32[]{:S(2)}, u32[]{:S(2)}) collective-permute-start(bf16[512,1536]{1,0:T(8,128)(2,1)} %dynamic-slice_bitcast_fusion.2), channel_id=1, source_target_pairs={{0,1},{1,0},{2,3},{3,2},{4,5},{5,4},{6,7},{7,6}} | collective-permute-start | bytes 4718600 | tf_op jit(solution)/shard_map/ppermute | solution.py:35
  40.4 1454.7 %all-gather.11.cloned.1.call-start = ((), (), s32[]{:S(2)}) async-start(), calls=%async_computation.10 | async-start | bytes 14155776 | tf_op jit(solution)/shard_map/all_gather | solution.py:423
  76.6 98.3 %collective-permute-start.3 = (bf16[384,1536]{1,0:T(8,128)(2,1)}, bf16[384,1536]{1,0:T(8,128)(2,1)}, u32[]{:S(2)}, u32[]{:S(2)}) collective-permute-start(bf16[384,1536]{1,0:T(8,128)(2,1)} %collective-permute-done.2), channel_id=1, source_target_pairs={{0,1},{1,0},{2,3},{3,2},{4,5},{5,4},{6,7},{7,6}} | collective-permute-start | bytes 3538952 | tf_op jit(solution)/shard_map/ppermute | solution.py:35
  166.6 45.9 %collective-permute-start.18 = (bf16[384,1536]{1,0:T(8,128)(2,1)}, bf16[384,1536]{1,0:T(8,128)(2,1)S(1)}, u32[]{:S(2)}, u32[]{:S(2)}) collective-permute-start(bf16[384,1536]{1,0:T(8,128)(2,1)} %get-tuple-element.204), channel_id=1, source_target_pairs={{0,4},{4,0},{2,6},{6,2},{1,5},{5,1},{3,7},{7,3}} | collective-permute-start | bytes 3538952 | tf_op jit(solution)/shard_map/ppermute | solution.py:31
  170.7 39.4 %collective-permute-start.16 = (bf16[384,1536]{1,0:T(8,128)(2,1)S(1)}, bf16[384,1536]{1,0:T(8,128)(2,1)S(1)}, u32[]{:S(2)}, u32[]{:S(2)}) collective-permute-start(bf16[384,1536]{1,0:T(8,128)(2,1)S(1)} %copy-done.46), channel_id=1, source_target_pairs={{0,2},{2,0},{4,6},{6,4},{1,3},{3,1},{5,7},{7,5}} | collective-permute-start | bytes 3538952 | tf_op jit(solution)/shard_map/ppermute | solution.py:27
  174.6 39.3 %collective-permute-start.15 = (bf16[384,1536]{1,0:T(8,128)(2,1)}, bf16[384,1536]{1,0:T(8,128)(2,1)S(1)}, u32[]{:S(2)}, u32[]{:S(2)}) collective-permute-start(bf16[384,1536]{1,0:T(8,128)(2,1)} %collective-permute-done.14), channel_id=1, source_target_pairs={{0,1},{1,0},{2,3},{3,2},{4,5},{5,4},{6,7},{7,6}} | collective-permute-start | bytes 3538952 | tf_op jit(solution)/shard_map/ppermute | solution.py:35
  174.9 41.5 %collective-permute-start.5 = (bf16[384,1536]{1,0:T(8,128)(2,1)}, bf16[384,1536]{1,0:T(8,128)(2,1)S(1)}, u32[]{:S(2)}, u32[]{:S(2)}) collective-permute-start(bf16[384,1536]{1,0:T(8,128)(2,1)} %collective-permute-done.4), channel_id=1, source_target_pairs={{0,1},{1,0},{2,3},{3,2},{4,5},{5,4},{6,7},{7,6}} | collective-permute-start | bytes 3538952 | tf_op jit(solution)/shard_map/ppermute | solution.py:35
  181.2 52.4 %collective-permute-start.8 = (bf16[384,1536]{1,0:T(8,128)(2,1)}, bf16[384,1536]{1,0:T(8,128)(2,1)S(1)}, u32[]{:S(2)}, u32[]{:S(2)}) collective-permute-start(bf16[384,1536]{1,0:T(8,128)(2,1)} %get-tuple-element.209), channel_id=1, source_target_pairs={{0,4},{4,0},{2,6},{6,2},{1,5},{5,1},{3,7},{7,3}} | collective-permute-start | bytes 3538952 | tf_op jit(solution)/shard_map/ppermute | solution.py:31
  212.5 46.5 %collective-permute-start.20 = (bf16[384,1536]{1,0:T(8,128)(2,1)S(1)}, bf16[384,1536]{1,0:T(8,128)(2,1)}, u32[]{:S(2)}, u32[]{:S(2)}) collective-permute-start(bf16[384,1536]{1,0:T(8,128)(2,1)S(1)} %copy-done.46), channel_id=1, source_target_pairs={{0,4},{4,0},{2,6},{6,2},{1,5},{5,1},{3,7},{7,3}} | collective-permute-start | bytes 3538952 | tf_op jit(solution)/shard_map/ppermute | solution.py:31
  214.0 45.6 %collective-permute-start.7 = (bf16[384,1536]{1,0:T(8,128)(2,1)}, bf16[384,1536]{1,0:T(8,128)(2,1)S(1)}, u32[]{:S(2)}, u32[]{:S(2)}) collective-permute-start(bf16[384,1536]{1,0:T(8,128)(2,1)} %collective-permute-done.6), channel_id=1, source_target_pairs={{0,1},{1,0},{2,3},{3,2},{4,5},{5,4},{6,7},{7,6}} | collective-permute-start | bytes 3538952 | tf_op jit(solution)/shard_map/ppermute | solution.py:35
  216.4 48.1 %collective-permute-start.19 = (bf16[384,1536]{1,0:T(8,128)(2,1)S(1)}, bf16[384,1536]{1,0:T(8,128)(2,1)S(1)}, u32[]{:S(2)}, u32[]{:S(2)}) collective-permute-start(bf16[384,1536]{1,0:T(8,128)(2,1)S(1)} %collective-permute-done.18), channel_id=1, source_target_pairs={{0,1},{1,0},{2,3},{3,2},{4,5},{5,4},{6,7},{7,6}} | collective-permute-start | bytes 3538952 | tf_op jit(solution)/shard_map/ppermute | solution.py:35
  233.6 50.7 %collective-permute-start.10 = (bf16[384,1536]{1,0:T(8,128)(2,1)}, bf16[384,1536]{1,0:T(8,128)(2,1)}, u32[]{:S(2)}, u32[]{:S(2)}) collective-permute-start(bf16[384,1536]{1,0:T(8,128)(2,1)} %collective-permute-done.2), channel_id=1, source_target_pairs={{0,4},{4,0},{2,6},{6,2},{1,5},{5,1},{3,7},{7,3}} | collective-permute-start | bytes 3538952 | tf_op jit(solution)/shard_map/ppermute | solution.py:31
  235.2 32.8 %collective-permute-start.9 = (bf16[384,1536]{1,0:T(8,128)(2,1)S(1)}, bf16[384,1536]{1,0:T(8,128)(2,1)S(1)}, u32[]{:S(2)}, u32[]{:S(2)}) collective-permute-start(bf16[384,1536]{1,0:T(8,128)(2,1)S(1)} %collective-permute-done.8), channel_id=1, source_target_pairs={{0,1},{1,0},{2,3},{3,2},{4,5},{5,4},{6,7},{7,6}} | collective-permute-start | bytes 3538952 | tf_op jit(solution)/shard_map/ppermute | solution.py:35
  259.6 49.4 %collective-permute-start.22 = (bf16[384,1536]{1,0:T(8,128)(2,1)}, bf16[384,1536]{1,0:T(8,128)(2,1)}, u32[]{:S(2)}, u32[]{:S(2)}) collective-permute-start(bf16[384,1536]{1,0:T(8,128)(2,1)} %collective-permute-done.14), channel_id=1, source_target_pairs={{0,4},{4,0},{2,6},{6,2},{1,5},{5,1},{3,7},{7,3}} | collective-permute-start | bytes 3538952 | tf_op jit(solution)/shard_map/ppermute | solution.py:31
  264.5 64.3 %collective-permute-start.21 = (bf16[384,1536]{1,0:T(8,128)(2,1)}, bf16[384,1536]{1,0:T(8,128)(2,1)}, u32[]{:S(2)}, u32[]{:S(2)}) collective-permute-start(bf16[384,1536]{1,0:T(8,128)(2,1)} %collective-permute-done.20), channel_id=1, source_target_pairs={{0,1},{1,0},{2,3},{3,2},{4,5},{5,4},{6,7},{7,6}} | collective-permute-start | bytes 3538952 | tf_op jit(solution)/shard_map/ppermute | solution.py:35
  268.0 66.0 %collective-permute-start.24 = (bf16[384,1536]{1,0:T(8,128)(2,1)}, bf16[384,1536]{1,0:T(8,128)(2,1)}, u32[]{:S(2)}, u32[]{:S(2)}) collective-permute-start(bf16[384,1536]{1,0:T(8,128)(2,1)} %collective-permute-done.20), channel_id=1, source_target_pairs={{0,2},{2,0},{4,6},{6,4},{1,3},{3,1},{5,7},{7,5}} | collective-permute-start | bytes 3538952 | tf_op jit(solution)/shard_map/ppermute | solution.py:27
  284.3 49.8 %collective-permute-start.11 = (bf16[384,1536]{1,0:T(8,128)(2,1)}, bf16[384,1536]{1,0:T(8,128)(2,1)}, u32[]{:S(2)}, u32[]{:S(2)}) collective-permute-start(bf16[384,1536]{1,0:T(8,128)(2,1)} %collective-permute-done.10), channel_id=1, source_target_pairs={{0,1},{1,0},{2,3},{3,2},{4,5},{5,4},{6,7},{7,6}} | collective-permute-start | bytes 3538952 | tf_op jit(solution)/shard_map/ppermute | solution.py:35
  287.8 54.5 %collective-permute-start.13 = (bf16[384,1536]{1,0:T(8,128)(2,1)S(1)}, bf16[384,1536]{1,0:T(8,128)(2,1)}, u32[]{:S(2)}, u32[]{:S(2)}) collective-permute-start(bf16[384,1536]{1,0:T(8,128)(2,1)S(1)} %collective-permute-done.12), channel_id=1, source_target_pairs={{0,1},{1,0},{2,3},{3,2},{4,5},{5,4},{6,7},{7,6}} | collective-permute-start | bytes 3538952 | tf_op jit(solution)/shard_map/ppermute | solution.py:35
  428.1 76.9 %collective-permute-start.28 = (bf16[512,1536]{1,0:T(8,128)(2,1)}, bf16[512,1536]{1,0:T(8,128)(2,1)}, u32[]{:S(2)}, u32[]{:S(2)}) collective-permute-start(bf16[512,1536]{1,0:T(8,128)(2,1)} %dynamic-slice_bitcast_fusion.1), channel_id=1, source_target_pairs={{0,1},{1,0},{2,3},{3,2},{4,5},{5,4},{6,7},{7,6}} | collective-permute-start | bytes 4718600 | tf_op jit(solution)/shard_map/ppermute | solution.py:35
  508.2 1101.3 %all-gather.13.cloned.1.call-start = ((), (), s32[]{:S(2)}) async-start(), calls=%async_computation.11 | async-start | bytes 14155776 | tf_op jit(solution)/shard_map/all_gather | solution.py:423
  761.9 863.9 %all-gather.15.cloned.1.call-start = ((), (), s32[]{:S(2)}) async-start(), calls=%async_computation.12 | async-start | bytes 14155776 | tf_op jit(solution)/shard_map/all_gather | solution.py:423
  870.1 772.5 %all-gather.17.cloned.1.call-start = ((), (), s32[]{:S(2)}) async-start(), calls=%async_computation.13 | async-start | bytes 14155776 | tf_op jit(solution)/shard_map/all_gather | solution.py:423
  978.6 831.6 %reduce-scatter.5.cloned.1.call-start = ((), (), s32[]{:S(2)}) async-start(), calls=%async_computation.9 | async-start | bytes 21233664 | tf_op jit(solution)/shard_map/reduce_scatter | solution.py:426
  1065.9 114.0 %all-to-all-start.3 = ((bf16[8,512,768]{2,1,0:T(8,128)(2,1)}), bf16[8,512,768]{2,1,0:T(8,128)(2,1)}, u32[]{:S(2)}, u32[]{:S(2)}) async-start(bf16[8,512,768]{2,1,0:T(8,128)(2,1)} %get-tuple-element.163), calls=%async_computation.5 | async-start | bytes 12582912 | tf_op jit(solution)/shard_map/all_to_all | solution.py:475
  1069.6 740.5 %reduce-scatter.3.cloned.1.call-start = ((), (), s32[]{:S(2)}) async-start(), calls=%async_computation.8 | async-start | bytes 21233664 | tf_op jit(solution)/shard_map/reduce_scatter | solution.py:426
  1121.9 190.9 %collective-permute-start.43 = (f32[512,1536]{1,0:T(8,128)}, f32[512,1536]{1,0:T(8,128)}, u32[]{:S(2)}, u32[]{:S(2)}) collective-permute-start(f32[512,1536]{1,0:T(8,128)} %get-tuple-element.147), channel_id=1, source_target_pairs={{0,1},{1,0},{2,3},{3,2},{4,5},{5,4},{6,7},{7,6}} | collective-permute-start | bytes 9437192 | tf_op jit(solution)/shard_map/ppermute | solution.py:35
  1135.6 48.1 %collective-permute-start.60 = (f32[384,768]{1,0:T(8,128)}, f32[384,768]{1,0:T(8,128)}, u32[]{:S(2)}, u32[]{:S(2)}) collective-permute-start(f32[384,768]{1,0:T(8,128)} %fusion.54), channel_id=1, source_target_pairs={{0,1},{1,0},{2,3},{3,2},{4,5},{5,4},{6,7},{7,6}} | collective-permute-start | bytes 3538952 | tf_op jit(solution)/shard_map/ppermute | solution.py:35
  1139.6 50.0 %collective-permute-start.63 = (f32[384,768]{1,0:T(8,128)}, f32[384,768]{1,0:T(8,128)S(1)}, u32[]{:S(2)}, u32[]{:S(2)}) collective-permute-start(f32[384,768]{1,0:T(8,128)} %fusion.46), channel_id=1, source_target_pairs={{0,1},{1,0},{2,3},{3,2},{4,5},{5,4},{6,7},{7,6}} | collective-permute-start | bytes 3538952 | tf_op jit(solution)/shard_map/ppermute | solution.py:35
  1162.7 29.9 %collective-permute-start.62 = (f32[384,768]{1,0:T(8,128)}, f32[384,768]{1,0:T(8,128)}, u32[]{:S(2)}, u32[]{:S(2)}) collective-permute-start(f32[384,768]{1,0:T(8,128)} %fusion.50), channel_id=1, source_target_pairs={{0,1},{1,0},{2,3},{3,2},{4,5},{5,4},{6,7},{7,6}} | collective-permute-start | bytes 3538952 | tf_op jit(solution)/shard_map/ppermute | solution.py:35
  1164.1 30.7 %collective-permute-start.37 = (f32[768,384]{1,0:T(8,128)}, f32[768,384]{1,0:T(8,128)}, u32[]{:S(2)}, u32[]{:S(2)}) collective-permute-start(f32[768,384]{1,0:T(8,128)} %fusion.102), channel_id=1, source_target_pairs={{0,1},{1,0},{2,3},{3,2},{4,5},{5,4},{6,7},{7,6}} | collective-permute-start | bytes 3538952 | tf_op jit(solution)/shard_map/ppermute | solution.py:35
  1180.0 148.0 %all-to-all-start.1 = ((bf16[8,512,768]{2,1,0:T(8,128)(2,1)}), bf16[8,512,768]{2,1,0:T(8,128)(2,1)}, u32[]{:S(2)}, u32[]{:S(2)}) async-start(bf16[8,512,768]{2,1,0:T(8,128)(2,1)} %get-tuple-element.159), calls=%async_computation.3 | async-start | bytes 12582912 | tf_op jit(solution)/shard_map/all_to_all | solution.py:475
  1183.7 133.6 %collective-permute-start.51 = (f32[512,1536]{1,0:T(8,128)}, f32[512,1536]{1,0:T(8,128)S(1)}, u32[]{:S(2)}, u32[]{:S(2)}) collective-permute-start(f32[512,1536]{1,0:T(8,128)} %get-tuple-element.150), channel_id=1, source_target_pairs={{0,1},{1,0},{2,3},{3,2},{4,5},{5,4},{6,7},{7,6}} | collective-permute-start | bytes 9437192 | tf_op jit(solution)/shard_map/ppermute | solution.py:35
  1192.7 115.9 %collective-permute-start.64 = (f32[384,768]{1,0:T(8,128)S(1)}, f32[384,768]{1,0:T(8,128)S(1)}, u32[]{:S(2)}, u32[]{:S(2)}) collective-permute-start(f32[384,768]{1,0:T(8,128)S(1)} %fusion.182), channel_id=1, source_target_pairs={{0,4},{4,0},{2,6},{6,2},{1,5},{5,1},{3,7},{7,3}} | collective-permute-start | bytes 3538952 | tf_op jit(solution)/shard_map/ppermute | solution.py:31
  1194.8 115.5 %collective-permute-start.41 = (f32[768,384]{1,0:T(8,128)S(1)}, f32[768,384]{1,0:T(8,128)S(1)}, u32[]{:S(2)}, u32[]{:S(2)}) collective-permute-start(f32[768,384]{1,0:T(8,128)S(1)} %fusion.128), channel_id=1, source_target_pairs={{0,2},{2,0},{4,6},{6,4},{1,3},{3,1},{5,7},{7,5}} | collective-permute-start | bytes 3538952 | tf_op jit(solution)/shard_map/ppermute | solution.py:27
  1203.6 257.8 %collective-permute-start.59 = (f32[384,768]{1,0:T(8,128)}, f32[384,768]{1,0:T(8,128)S(1)}, u32[]{:S(2)}, u32[]{:S(2)}) collective-permute-start(f32[384,768]{1,0:T(8,128)} %fusion.58), channel_id=1, source_target_pairs={{0,1},{1,0},{2,3},{3,2},{4,5},{5,4},{6,7},{7,6}} | collective-permute-start | bytes 3538952 | tf_op jit(solution)/shard_map/ppermute | solution.py:35
  1308.6 153.2 %collective-permute-start.61 = (f32[384,768]{1,0:T(8,128)}, f32[384,768]{1,0:T(8,128)}, u32[]{:S(2)}, u32[]{:S(2)}) collective-permute-start(f32[384,768]{1,0:T(8,128)} %fusion.176), channel_id=1, source_target_pairs={{0,4},{4,0},{2,6},{6,2},{1,5},{5,1},{3,7},{7,3}} | collective-permute-start | bytes 3538952 | tf_op jit(solution)/shard_map/ppermute | solution.py:31
  1310.2 153.2 %collective-permute-start.65 = (f32[384,768]{1,0:T(8,128)}, f32[384,768]{1,0:T(8,128)}, u32[]{:S(2)}, u32[]{:S(2)}) collective-permute-start(f32[384,768]{1,0:T(8,128)} %add.654), channel_id=1, source_target_pairs={{0,2},{2,0},{4,6},{6,4},{1,3},{3,1},{5,7},{7,5}} | collective-permute-start | bytes 3538952 | tf_op jit(solution)/shard_map/ppermute | solution.py:27
  1328.0 129.3 %all-to-all-start = ((bf16[8,512,768]{2,1,0:T(8,128)(2,1)}), bf16[8,512,768]{2,1,0:T(8,128)(2,1)}, u32[]{:S(2)}, u32[]{:S(2)}) async-start(bf16[8,512,768]{2,1,0:T(8,128)(2,1)} %get-tuple-element.157), calls=%async_computation.2 | async-start | bytes 12582912 | tf_op jit(solution)/shard_map/all_to_all | solution.py:475
  1337.3 131.4 %collective-permute-start.53 = (f32[768,384]{1,0:T(8,128)}, f32[768,384]{1,0:T(8,128)}, u32[]{:S(2)}, u32[]{:S(2)}) collective-permute-start(f32[768,384]{1,0:T(8,128)} %fusion.70), channel_id=1, source_target_pairs={{0,1},{1,0},{2,3},{3,2},{4,5},{5,4},{6,7},{7,6}} | collective-permute-start | bytes 3538952 | tf_op jit(solution)/shard_map/ppermute | solution.py:35
  1366.7 107.4 %collective-permute-start.56 = (f32[768,384]{1,0:T(8,128)}, f32[768,384]{1,0:T(8,128)}, u32[]{:S(2)}, u32[]{:S(2)}) collective-permute-start(f32[768,384]{1,0:T(8,128)} %fusion.62), channel_id=1, source_target_pairs={{0,1},{1,0},{2,3},{3,2},{4,5},{5,4},{6,7},{7,6}} | collective-permute-start | bytes 3538952 | tf_op jit(solution)/shard_map/ppermute | solution.py:35
  1457.2 97.5 %all-to-all-start.2 = ((bf16[8,512,768]{2,1,0:T(8,128)(2,1)}), bf16[8,512,768]{2,1,0:T(8,128)(2,1)}, u32[]{:S(2)}, u32[]{:S(2)}) async-start(bf16[8,512,768]{2,1,0:T(8,128)(2,1)} %get-tuple-element.161), calls=%async_computation.4 | async-start | bytes 12582912 | tf_op jit(solution)/shard_map/all_to_all | solution.py:475
  1461.4 180.7 %collective-permute-start.36 = (f32[768,384]{1,0:T(8,128)}, f32[768,384]{1,0:T(8,128)}, u32[]{:S(2)}, u32[]{:S(2)}) collective-permute-start(f32[768,384]{1,0:T(8,128)} %fusion.106), channel_id=1, source_target_pairs={{0,1},{1,0},{2,3},{3,2},{4,5},{5,4},{6,7},{7,6}} | collective-permute-start | bytes 3538952 | tf_op jit(solution)/shard_map/ppermute | solution.py:35
  1461.8 180.3 %collective-permute-start.38 = (f32[768,384]{1,0:T(8,128)}, f32[768,384]{1,0:T(8,128)}, u32[]{:S(2)}, u32[]{:S(2)}) collective-permute-start(f32[768,384]{1,0:T(8,128)} %fusion.122), channel_id=1, source_target_pairs={{0,2},{2,0},{4,6},{6,4},{1,3},{3,1},{5,7},{7,5}} | collective-permute-start | bytes 3538952 | tf_op jit(solution)/shard_map/ppermute | solution.py:27
  1484.0 179.0 %collective-permute-start.42 = (f32[768,384]{1,0:T(8,128)}, f32[768,384]{1,0:T(8,128)}, u32[]{:S(2)}, u32[]{:S(2)}) collective-permute-start(f32[768,384]{1,0:T(8,128)} %add.631), channel_id=1, source_target_pairs={{0,4},{4,0},{2,6},{6,2},{1,5},{5,1},{3,7},{7,3}} | collective-permute-start | bytes 3538952 | tf_op jit(solution)/shard_map/ppermute | solution.py:31
  1488.5 66.2 %collective-permute-start.73 = (bf16[512,1536]{1,0:T(8,128)(2,1)S(1)}, bf16[512,1536]{1,0:T(8,128)(2,1)}, u32[]{:S(2)}, u32[]{:S(2)}) collective-permute-start(bf16[512,1536]{1,0:T(8,128)(2,1)S(1)} %get-tuple-element.172), channel_id=1, source_target_pairs={{0,1},{1,0},{2,3},{3,2},{4,5},{5,4},{6,7},{7,6}} | collective-permute-start | bytes 4718600 | tf_op jit(solution)/shard_map/ppermute | solution.py:35
  1491.5 112.6 %collective-permute-start.57 = (f32[768,384]{1,0:T(8,128)}, f32[768,384]{1,0:T(8,128)}, u32[]{:S(2)}, u32[]{:S(2)}) collective-permute-start(f32[768,384]{1,0:T(8,128)} %fusion.164), channel_id=1, source_target_pairs={{0,4},{4,0},{2,6},{6,2},{1,5},{5,1},{3,7},{7,3}} | collective-permute-start | bytes 3538952 | tf_op jit(solution)/shard_map/ppermute | solution.py:31
  1554.7 109.3 %collective-permute-start.52 = (f32[768,384]{1,0:T(8,128)}, f32[768,384]{1,0:T(8,128)}, u32[]{:S(2)}, u32[]{:S(2)}) collective-permute-start(f32[768,384]{1,0:T(8,128)} %fusion.74), channel_id=1, source_target_pairs={{0,1},{1,0},{2,3},{3,2},{4,5},{5,4},{6,7},{7,6}} | collective-permute-start | bytes 3538952 | tf_op jit(solution)/shard_map/ppermute | solution.py:35
  1604.2 66.6 %collective-permute-start.74 = (bf16[1024,1536]{1,0:T(8,128)(2,1)}, bf16[1024,1536]{1,0:T(8,128)(2,1)}, u32[]{:S(2)}, u32[]{:S(2)}) collective-permute-start(bf16[1024,1536]{1,0:T(8,128)(2,1)} %constant_dynamic-update-slice_fusion), channel_id=1, source_target_pairs={{0,4},{2,6},{5,1},{7,3}} | collective-permute-start | bytes 9437192 | tf_op jit(solution)/shard_map/ppermute | solution.py:534
  1664.0 28.8 %collective-permute-start.49 = (f32[768,384]{1,0:T(8,128)S(1)}, f32[768,384]{1,0:T(8,128)S(1)}, u32[]{:S(2)}, u32[]{:S(2)}) collective-permute-start(f32[768,384]{1,0:T(8,128)S(1)} %copy-done.160), channel_id=1, source_target_pairs={{0,2},{2,0},{4,6},{6,4},{1,3},{3,1},{5,7},{7,5}} | collective-permute-start | bytes 3538952 | tf_op jit(solution)/shard_map/ppermute | solution.py:27
  1665.5 52.7 %collective-permute-start.58 = (f32[768,384]{1,0:T(8,128)S(1)}, f32[768,384]{1,0:T(8,128)}, u32[]{:S(2)}, u32[]{:S(2)}) collective-permute-start(f32[768,384]{1,0:T(8,128)S(1)} %add.647), channel_id=1, source_target_pairs={{0,2},{2,0},{4,6},{6,4},{1,3},{3,1},{5,7},{7,5}} | collective-permute-start | bytes 3538952 | tf_op jit(solution)/shard_map/ppermute | solution.py:27
  1666.0 165.6 %collective-permute-start.72 = (f32[768,1536]{1,0:T(8,128)}, f32[768,1536]{1,0:T(8,128)}, u32[]{:S(2)}, u32[]{:S(2)}) collective-permute-start(f32[768,1536]{1,0:T(8,128)} %add_add_fusion.4.refs_0_), channel_id=1, source_target_pairs={{0,1},{1,0},{2,3},{3,2},{4,5},{5,4},{6,7},{7,6}} | collective-permute-start | bytes 14155784 | tf_op jit(solution)/shard_map/ppermute | solution.py:35
  1670.8 53.5 %collective-permute-start.66 = (f32[768,384]{1,0:T(8,128)S(1)}, f32[768,384]{1,0:T(8,128)S(1)}, u32[]{:S(2)}, u32[]{:S(2)}) collective-permute-start(f32[768,384]{1,0:T(8,128)S(1)} %fusion.119.refs_0_), channel_id=1, source_target_pairs={{0,1},{1,0},{2,3},{3,2},{4,5},{5,4},{6,7},{7,6}} | collective-permute-start | bytes 3538952 | tf_op jit(solution)/shard_map/ppermute | solution.py:35
  1691.0 136.8 %collective-permute-start.75 = (bf16[1024,1536]{1,0:T(8,128)(2,1)}, bf16[1024,1536]{1,0:T(8,128)(2,1)}, u32[]{:S(2)}, u32[]{:S(2)}) collective-permute-start(bf16[1024,1536]{1,0:T(8,128)(2,1)} %get-tuple-element.170), channel_id=1, source_target_pairs={{0,2},{2,0},{4,6},{6,4},{1,3},{3,1},{5,7},{7,5}} | collective-permute-start | bytes 9437192 | tf_op jit(solution)/shard_map/ppermute | solution.py:27
  1692.8 117.3 %collective-permute-start.46 = (f32[768,384]{1,0:T(8,128)S(1)}, f32[768,384]{1,0:T(8,128)}, u32[]{:S(2)}, u32[]{:S(2)}) collective-permute-start(f32[768,384]{1,0:T(8,128)S(1)} %copy-done.158), channel_id=1, source_target_pairs={{0,2},{2,0},{4,6},{6,4},{1,3},{3,1},{5,7},{7,5}} | collective-permute-start | bytes 3538952 | tf_op jit(solution)/shard_map/ppermute | solution.py:27
  1718.2 91.9 %collective-permute-start.50 = (f32[768,384]{1,0:T(8,128)}, f32[768,384]{1,0:T(8,128)}, u32[]{:S(2)}, u32[]{:S(2)}) collective-permute-start(f32[768,384]{1,0:T(8,128)} %add.639), channel_id=1, source_target_pairs={{0,4},{4,0},{2,6},{6,2},{1,5},{5,1},{3,7},{7,3}} | collective-permute-start | bytes 3538952 | tf_op jit(solution)/shard_map/ppermute | solution.py:31
  1725.4 91.5 %collective-permute-start.68 = (f32[768,384]{1,0:T(8,128)}, f32[768,384]{1,0:T(8,128)S(1)}, u32[]{:S(2)}, u32[]{:S(2)}) collective-permute-start(f32[768,384]{1,0:T(8,128)} %fusion.155.refs_2_), channel_id=1, source_target_pairs={{0,1},{1,0},{2,3},{3,2},{4,5},{5,4},{6,7},{7,6}} | collective-permute-start | bytes 3538952 | tf_op jit(solution)/shard_map/ppermute | solution.py:35
  1810.1 33.0 %collective-permute-start.71 = (f32[768,768]{1,0:T(8,128)}, f32[768,768]{1,0:T(8,128)S(1)}, u32[]{:S(2)}, u32[]{:S(2)}) collective-permute-start(f32[768,768]{1,0:T(8,128)} %reduce-scatter.5.cloned.1.call-done.ob_ref), channel_id=1, source_target_pairs={{0,1},{1,0},{2,3},{3,2},{4,5},{5,4},{6,7},{7,6}} | collective-permute-start | bytes 7077896 | tf_op jit(solution)/shard_map/ppermute | solution.py:35
  1810.1 33.0 %collective-permute-start.70 = (f32[768,768]{1,0:T(8,128)}, f32[768,768]{1,0:T(8,128)}, u32[]{:S(2)}, u32[]{:S(2)}) collective-permute-start(f32[768,768]{1,0:T(8,128)} %reduce-scatter.3.cloned.1.call-done.oa_ref), channel_id=1, source_target_pairs={{0,1},{1,0},{2,3},{3,2},{4,5},{5,4},{6,7},{7,6}} | collective-permute-start | bytes 7077896 | tf_op jit(solution)/shard_map/ppermute | solution.py:35
  (201 other events, 3712.1 us)
Sparse Core Ops, SparseCore 0:
  16.2 129.7 all-gather.6
  147.9 51.3 all-gather.8
  508.3 67.0 all-gather.10
  762.0 66.8 all-gather.12
  870.3 66.8 all-gather.14
  978.7 66.8 all-gather.16
  1066.0 228.3 reduce-scatter.4
  1298.0 228.6 reduce-scatter.2

commit v6 on v5

--- a/solution.py
+++ b/solution.py
@@ -33,10 +33,6 @@
 
 def pp_d(v):
     return lax.ppermute(v, 'data', SWAP_D)
-
-
-def rms_norm(values):
-    return values * lax.rsqrt(jnp.mean(values * values, axis=-1, keepdims=True) + EPS_NORM)
 
 
 def dot(a, b, dims):
@@ -140,15 +136,13 @@
 
 def attn_bwd_body(*refs):
     q_ref, ko_ref, ks_ref, vo_ref, vs_ref, do_ref, lse_ref = refs[:7]
-    dq_ref, dko_ref, dks_ref, dvo_ref, dvs_ref = refs[-5:]
+    dq_ref, down_ref, dsib_ref = refs[-3:]
     tk = ko_ref.shape[0]
     k = jnp.concatenate([ko_ref[...], ks_ref[...]], axis=0)
     v = jnp.concatenate([vo_ref[...], vs_ref[...]], axis=0)
-    tq = q_ref.shape[0]
-    chunk = 256
-    low = pair_masks(chunk)
-    for i in range(tq // chunk):
-        rows = slice(i * chunk, (i + 1) * chunk)
+    low = pair_masks(CHUNK)
+    for i in range(q_ref.shape[0] // CHUNK):
+        rows = slice(i * CHUNK, (i + 1) * CHUNK)
         q = q_ref[rows, :]
         do = do_ref[rows, :]
         dqs = []
@@ -163,16 +157,12 @@
             ds = (p * (dp - delta)).astype(BF16)
             dv = nn(p.astype(BF16), dom)
             dk = nn(ds, qm) * SCALE
-            if i == 0 and h == 0:
-                dvo_ref[...] = dv[:tk]
-                dvs_ref[...] = dv[tk:]
-                dko_ref[...] = dk[:tk]
-                dks_ref[...] = dk[tk:]
-            else:
-                dvo_ref[...] += dv[:tk]
-                dvs_ref[...] += dv[tk:]
-                dko_ref[...] += dk[:tk]
-                dks_ref[...] += dk[tk:]
+            for n, grad in enumerate((dk, dv)):
+                for ref, part in ((down_ref, grad[:tk]), (dsib_ref, grad[tk:])):
+                    if i == 0 and h == 0:
+                        ref[n] = part
+                    else:
+                        ref[n] += part
             dqs.append(tn(k, ds)[h * HEAD_DIM:(h + 1) * HEAD_DIM, :] * SCALE)
         dq_ref[0, rows, :] = jnp.concatenate(dqs, axis=0).T.astype(BF16)
 
@@ -187,6 +177,7 @@
 
     flops = 5 * 2 * tq * (2 * tk) * 256 * (width // HEAD_DIM)
     kblk = pl.BlockSpec((tk, 128), col(0))
+    both = pl.BlockSpec((2, tk, 128), lambda j: (0, 0, j))
     extra = [] if hist is None else [hist]
     return pl.pallas_call(
         attn_bwd_body,
@@ -197,9 +188,9 @@
                   pl.BlockSpec((tq, 128), col(0)),
                   pl.BlockSpec((1, 2, tq), lambda j: (j, 0, 0))]
         + [pl.BlockSpec(memory_space=pl.ANY)] * len(extra),
-        out_specs=[pl.BlockSpec((1, tq, 128), lambda j: (layer, 0, j)), kblk, kblk, kblk, kblk],
+        out_specs=[pl.BlockSpec((1, tq, 128), lambda j: (layer, 0, j)), both, both],
         out_shape=[jax.ShapeDtypeStruct((layers, tq, width), BF16)]
-        + [jax.ShapeDtypeStruct((tk, width), F32)] * 4,
+        + [jax.ShapeDtypeStruct((2, tk, width), F32)] * 2,
         input_output_aliases={7: 0} if extra else {},
         compiler_params=pltpu.CompilerParams(dimension_semantics=('arbitrary',),
                                              vmem_limit_bytes=VMEM_ALL),
@@ -209,23 +200,145 @@
     )(q, kv, kv_s, kv, kv_s, d_ctx, lse, *extra)
 
 
+def kv_body(*refs):
+    x_ref, e_ref, w_ref = refs[:3]
+    kv_ref, u_ref = refs[-2:]
+
+    @pl.when(pl.program_id(0) == 0)
+    def _():
+        s = x_ref[...].astype(F32) + e_ref[...]
+        u_ref[0] = (s * lax.rsqrt(jnp.mean(s * s, axis=-1, keepdims=True) + EPS_NORM)).astype(BF16)
+
+    for rows in ROWS:
+        kv_ref[rows, :] = nt(u_ref[0, rows, :], w_ref[...]).astype(BF16)
+
+
+def norm_kv(x, e, wkv, layer, layers, hist):
+    t, dim = x.shape
+    width = wkv.shape[0]
+    blk = 1024
+    extra = [] if hist is None else [hist]
+    return pl.pallas_call(
+        kv_body,
+        grid=(width // blk,),
+        in_specs=[pl.BlockSpec((t, dim), lambda j: (0, 0)), pl.BlockSpec((1, dim), lambda j: (0, 0)),
+                  pl.BlockSpec((blk, dim), lambda j: (j, 0))] + [pl.BlockSpec(memory_space=pl.ANY)] * len(extra),
+        out_specs=[pl.BlockSpec((t, blk), lambda j: (0, j)), pl.BlockSpec((1, t, dim), lambda j: (layer, 0, 0))],
+        out_shape=[jax.ShapeDtypeStruct((t, width), BF16), jax.ShapeDtypeStruct((layers, t, dim), BF16)],
+        input_output_aliases={3: 1} if extra else {},
+        compiler_params=pltpu.CompilerParams(dimension_semantics=('arbitrary',), vmem_limit_bytes=VMEM_ALL),
+        cost_estimate=pl.CostEstimate(flops=2 * t * dim * width, bytes_accessed=2 * (dim * width + t * width + 2 * t * dim),
+                                      transcendentals=t),
+        name='norm_kv',
+    )(x, e, wkv, *extra)
+
+
+def d_kv_body(*refs):
+    acc0_ref, x_ref, e_ref, mid_ref, own_ref, recv_ref, w_ref = refs[:7]
+    dk_ref, dv_ref, prev_ref, acc_ref = refs[-4:]
+    j = pl.program_id(0)
+
+    @pl.when(j == 0)
+    def _():
+        acc_ref[...] = acc0_ref[...]
+
+    grad = (own_ref[0] + recv_ref[0]).astype(BF16)
+    half = grad.shape[1]
+    for n, ref in enumerate((dk_ref, dv_ref)):
+        for part in range(2):
+            @pl.when(j == 2 * n + part)
+            def _():
+                ref[0, :, part * half:(part + 1) * half] = grad
+
+    for rows in ROWS:
+        acc_ref[rows, :] += nn(grad[rows, :], w_ref[...])
+
+    @pl.when(j == pl.num_programs(0) - 1)
+    def _():
+        dn = acc_ref[...].astype(BF16).astype(F32)
+        s = x_ref[...].astype(F32) + e_ref[...]
+        inv = lax.rsqrt(jnp.mean(s * s, axis=-1, keepdims=True) + EPS_NORM)
+        proj = jnp.mean(s * dn, axis=-1, keepdims=True)
+        prev_ref[...] = (mid_ref[0].astype(F32) + inv * dn - s * (inv * inv * inv * proj)).astype(BF16)
+
+
+def d_kv(acc0, x, e, mid_hist, own, recv, wkv, layer, layers, dk_hist, dv_hist):
+    t, dim = x.shape
+    half = dim // 2
+    whole = pl.BlockSpec((t, dim), lambda j: (0, 0))
+    slab = pl.BlockSpec((1, t, dim), lambda j: (layer, 0, 0))
+    gblk = pl.BlockSpec((1, t, half), lambda j: (j // 2, 0, j % 2))
+    extra = [] if dk_hist is None else [dk_hist, dv_hist]
+    return pl.pallas_call(
+        d_kv_body,
+        grid=(4,),
+        in_specs=[whole, whole, pl.BlockSpec((1, dim), lambda j: (0, 0)), slab, gblk, gblk,
+                  pl.BlockSpec((half, dim), lambda j: (j, 0))] + [pl.BlockSpec(memory_space=pl.ANY)] * len(extra),
+        out_specs=[slab, slab, whole],
+        out_shape=[jax.ShapeDtypeStruct((layers, t, dim), BF16)] * 2 + [jax.ShapeDtypeStruct((t, dim), BF16)],
+        scratch_shapes=[pltpu.VMEM((t, dim), F32)],
+        input_output_aliases={7: 0, 8: 1} if extra else {},
+        compiler_params=pltpu.CompilerParams(dimension_semantics=('arbitrary',), vmem_limit_bytes=VMEM_ALL),
+        cost_estimate=pl.CostEstimate(flops=4 * t * dim * dim, bytes_accessed=4 * dim * dim + 20 * t * dim, transcendentals=t),
+        name='d_kv',
+    )(acc0, x, e, mid_hist, own, recv, wkv, *extra)
+
+
+def terms_body(added, *refs):
+    lhs, rhs, recv, outs = refs[:4], (refs[4], refs[4], refs[4], refs[5]), refs[6:6 + 4 * added], refs[-4:]
+    r, kind = pl.program_id(0), pl.program_id(1)
+    for n in range(4):
+        @pl.when(kind == n)
+        def _():
+            val = tn(lhs[n][...], rhs[n][...])
+            for c in range(2):
+                @pl.when(r == c)
+                def _():
+                    slot = 2 * c + n // 2
+                    outs[slot][0] = val + recv[slot][0] if added else val
+
+
+def terms(dq, dk, dv, ctx, u_half, mid_half, chips, recv):
+    tokens, dim = dq.shape
+    hid = dim // 4
+    half_d = u_half.shape[1]
+    first, second = chips
+    whole = pl.BlockSpec((tokens, half_d), lambda r, kind: (0, 0))
+    src = pl.BlockSpec((tokens, hid), lambda r, kind: (0, first + r * (second - first)))
+    slots = [pl.BlockSpec((1, hid, half_d), lambda r, kind, at=2 * n: (jnp.clip(4 * r + kind - at, 0, 1), 0, 0))
+             for n in range(4)]
+    out = pl.pallas_call(
+        functools.partial(terms_body, len(recv) // 4),
+        grid=(2, 4),
+        in_specs=[src] * 4 + [whole] * 2 + slots[:len(recv)],
+        out_specs=slots,
+        out_shape=[jax.ShapeDtypeStruct((2, hid, half_d), F32)] * 4,
+        compiler_params=pltpu.CompilerParams(dimension_semantics=('arbitrary', 'arbitrary'), vmem_limit_bytes=VMEM_ALL),
+        cost_estimate=pl.CostEstimate(flops=16 * tokens * hid * half_d, bytes_accessed=24 * tokens * hid, transcendentals=0),
+    )(dq, dk, dv, ctx, u_half, mid_half, *recv)
+    return {first: out[:2], second: out[2:]}
+
+
 GELU_C = 0.7978845608028654
 GELU_A = 0.044715
 BLOCK_F = 768
-SUB_F = 768
 ROWS = (slice(0, 256), slice(256, 512))
 
 
 def mlp_fwd_body(*refs):
-    h_ref, w1_ref, w2_ref = refs[:3]
-    z_ref, g_ref, x_ref, m_ref, acc_ref = refs[-5:]
+    x0_ref, e_ref, ctx_ref, wo_ref, w1_ref, w2_ref = refs[:6]
+    z_ref, g_ref, x_ref, h_ref, m_ref, acc_ref = refs[-6:]
     j = pl.program_id(0)
 
     @pl.when(j == 0)
     def _():
-        hf = h_ref[...].astype(F32)
-        acc_ref[...] = hf
-        m_ref[0] = (hf * lax.rsqrt(jnp.mean(hf * hf, axis=-1, keepdims=True) + EPS_NORM)).astype(BF16)
+        for rows in ROWS:
+            s = x0_ref[rows, :].astype(F32) + e_ref[...]
+            h = (s + nn(ctx_ref[0, rows, :], wo_ref[...])).astype(BF16)
+            h_ref[rows, :] = h
+            hf = h.astype(F32)
+            acc_ref[rows, :] = hf
+            m_ref[0, rows, :] = (hf * lax.rsqrt(jnp.mean(hf * hf, axis=-1, keepdims=True) + EPS_NORM)).astype(BF16)
 
     for rows in ROWS:
         z = nt(m_ref[0, rows, :], w1_ref[...]).astype(BF16)
@@ -242,43 +355,48 @@
         x_ref[...] = acc_ref[...].astype(BF16)
 
 
-def mlp_fwd(h, w1t, w2, layer, layers, hist):
-    t, dim = h.shape
+def mlp_fwd(x, e, ctx_hist, wo, w1t, w2, layer, layers, hist):
+    t, dim = x.shape
     hidden = w2.shape[0]
     whole = pl.BlockSpec((t, dim), lambda j: (0, 0))
+    slab = pl.BlockSpec((1, t, dim), lambda j: (layer, 0, 0))
     wblk = pl.BlockSpec((BLOCK_F, dim), lambda j: (j, 0))
     extra = [] if hist is None else [hist]
     return pl.pallas_call(
         mlp_fwd_body,
         grid=(hidden // BLOCK_F,),
-        in_specs=[whole, wblk, wblk] + [pl.BlockSpec(memory_space=pl.ANY)] * len(extra),
+        in_specs=[whole, pl.BlockSpec((1, dim), lambda j: (0, 0)), slab, pl.BlockSpec((dim, dim), lambda j: (0, 0)), wblk, wblk]
+        + [pl.BlockSpec(memory_space=pl.ANY)] * len(extra),
         out_specs=[pl.BlockSpec((t, BLOCK_F), lambda j: (0, j)),
-                   pl.BlockSpec((1, t, BLOCK_F), lambda j: (j, 0, 0)), whole,
-                   pl.BlockSpec((1, t, dim), lambda j: (layer, 0, 0))],
+                   pl.BlockSpec((1, t, BLOCK_F), lambda j: (j, 0, 0)), whole, whole, slab],
         out_shape=[jax.ShapeDtypeStruct((t, hidden), BF16),
                    jax.ShapeDtypeStruct((hidden // BLOCK_F, t, BLOCK_F), BF16),
-                   jax.ShapeDtypeStruct((t, dim), BF16),
+                   jax.ShapeDtypeStruct((t, dim), BF16), jax.ShapeDtypeStruct((t, dim), BF16),
                    jax.ShapeDtypeStruct((layers, t, dim), BF16)],
         scratch_shapes=[pltpu.VMEM((t, dim), F32)],
-        input_output_aliases={3: 3} if extra else {},
+        input_output_aliases={6: 4} if extra else {},
         compiler_params=pltpu.CompilerParams(dimension_semantics=('arbitrary',), vmem_limit_bytes=VMEM_ALL),
         cost_estimate=pl.CostEstimate(flops=4 * t * dim * hidden, bytes_accessed=4 * dim * hidden + 4 * t * hidden,
                                       transcendentals=t * hidden),
         name='mlp_fwd',
-    )(h, w1t, w2, *extra)
+    )(x, e, ctx_hist, wo, w1t, w2, *extra)
+
+
+BLOCK_B = 1024
+SUB_B = 512
 
 
 def mlp_bwd_body(*refs):
-    d_ref, h_ref, z_ref, w1_ref, w2_ref = refs[:5]
-    up_ref, mid_ref, acc_ref = refs[-3:]
+    d_ref, h_ref, z_ref, wo_ref, w1_ref, w2_ref = refs[:6]
+    up_ref, mid_ref, dctx_ref, acc_ref = refs[-4:]
     j = pl.program_id(0)
 
     @pl.when(j == 0)
     def _():
         acc_ref[...] = jnp.zeros_like(acc_ref)
 
-    for i in range(0, BLOCK_F, SUB_F):
-        cols = slice(i, i + SUB_F)
+    for i in range(0, BLOCK_B, SUB_B):
+        cols = slice(i, i + SUB_B)
         for rows in ROWS:
             da = nt(d_ref[rows, :], w2_ref[cols, :]).astype(BF16).astype(F32)
             zf = z_ref[rows, cols].astype(F32)
@@ -291,34 +409,37 @@
 
     @pl.when(j == pl.num_programs(0) - 1)
     def _():
-        dn = acc_ref[...].astype(BF16).astype(F32)
-        hf = h_ref[...].astype(F32)
-        inv = lax.rsqrt(jnp.mean(hf * hf, axis=-1, keepdims=True) + EPS_NORM)
-        proj = jnp.mean(hf * dn, axis=-1, keepdims=True)
-        mid_ref[0] = (d_ref[...].astype(F32) + inv * dn - hf * (inv * inv * inv * proj)).astype(BF16)
-
-
-def mlp_bwd(d_next, h, z, w1t, w2, layer, layers, hist, mid_hist):
+        for rows in ROWS:
+            dn = acc_ref[rows, :].astype(BF16).astype(F32)
+            hf = h_ref[rows, :].astype(F32)
+            inv = lax.rsqrt(jnp.mean(hf * hf, axis=-1, keepdims=True) + EPS_NORM)
+            proj = jnp.mean(hf * dn, axis=-1, keepdims=True)
+            mid = (d_ref[rows, :].astype(F32) + inv * dn - hf * (inv * inv * inv * proj)).astype(BF16)
+            mid_ref[0, rows, :] = mid
+            dctx_ref[rows, :] = nt(mid, wo_ref[...]).astype(BF16)
+
+
+def mlp_bwd(d_next, h, z, wo, w1t, w2, layer, layers, hist, mid_hist):
     t, dim = h.shape
     hidden = w2.shape[0]
     whole = pl.BlockSpec((t, dim), lambda j: (0, 0))
-    wblk = pl.BlockSpec((BLOCK_F, dim), lambda j: (j, 0))
-    hspec = pl.BlockSpec((1, t, BLOCK_F), lambda j: (layer, 0, j))
+    wblk = pl.BlockSpec((BLOCK_B, dim), lambda j: (j, 0))
     extra = [] if hist is None else [hist, mid_hist]
     return pl.pallas_call(
         mlp_bwd_body,
-        grid=(hidden // BLOCK_F,),
-        in_specs=[whole, whole, pl.BlockSpec((t, BLOCK_F), lambda j: (0, j)), wblk, wblk]
+        grid=(hidden // BLOCK_B,),
+        in_specs=[whole, whole, pl.BlockSpec((t, BLOCK_B), lambda j: (0, j)), pl.BlockSpec((dim, dim), lambda j: (0, 0)), wblk, wblk]
         + [pl.BlockSpec(memory_space=pl.ANY)] * len(extra),
-        out_specs=[hspec, pl.BlockSpec((1, t, dim), lambda j: (layer, 0, 0))],
-        out_shape=[jax.ShapeDtypeStruct((layers, t, hidden), BF16), jax.ShapeDtypeStruct((layers, t, dim), BF16)],
+        out_specs=[pl.BlockSpec((1, t, BLOCK_B), lambda j: (layer, 0, j)), pl.BlockSpec((1, t, dim), lambda j: (layer, 0, 0)), whole],
+        out_shape=[jax.ShapeDtypeStruct((layers, t, hidden), BF16), jax.ShapeDtypeStruct((layers, t, dim), BF16),
+                   jax.ShapeDtypeStruct((t, dim), BF16)],
         scratch_shapes=[pltpu.VMEM((t, dim), F32)],
-        input_output_aliases={5: 0, 6: 1} if extra else {},
+        input_output_aliases={6: 0, 7: 1} if extra else {},
         compiler_params=pltpu.CompilerParams(dimension_semantics=('arbitrary',), vmem_limit_bytes=VMEM_ALL),
         cost_estimate=pl.CostEstimate(flops=4 * t * dim * hidden, bytes_accessed=4 * dim * hidden + 4 * t * hidden,
                                       transcendentals=t * hidden),
         name='mlp_bwd',
-    )(d_next, h, z, w1t, w2, *extra)
+    )(d_next, h, z, wo, w1t, w2, *extra)
 
 
 def join_body(count, core_ref, *refs):
@@ -341,18 +462,31 @@
     )(core.reshape(1), *own, *other)
 
 
-def join(core, own, other, axes, parts):
-    in_specs, out_specs, out_shape = [], [], []
-    for v, axis in zip(own, axes):
-        rows, cols = v.shape[0], v.shape[1] // parts
-        in_specs.append(pl.BlockSpec((rows, cols), lambda i, j, c: (0, j)))
-        if axis == 0:
-            out_shape.append(jax.ShapeDtypeStruct((2 * rows, v.shape[1]), v.dtype))
-            out_specs.append(pl.BlockSpec((rows, cols), lambda i, j, c: ((c[0] + i) % 2, j)))
-        else:
-            out_shape.append(jax.ShapeDtypeStruct((rows, 2 * v.shape[1]), v.dtype))
-            out_specs.append(pl.BlockSpec((rows, cols), lambda i, j, c, parts=parts: (0, ((c[0] + i) % 2) * parts + j)))
-    return join_call(core, functools.partial(join_body, len(own)), (2, parts), own, other, in_specs, out_specs, out_shape)
+def join(core, own, other):
+    rows, cols = own.shape[0], own.shape[1] // 4
+    block = pl.BlockSpec((rows, cols), lambda i, j, c: (0, j))
+    return join_call(core, functools.partial(join_body, 1), (2, 4), [own], [other], [block],
+                     pl.BlockSpec((rows, cols), lambda i, j, c: ((c[0] + i) % 2, j)),
+                     jax.ShapeDtypeStruct((2 * rows, own.shape[1]), F32))
+
+
+def join_attn_body(core_ref, own_a, own_b, sib_a, sib_b, q_ref, k_ref, v_ref, o_ref):
+    for i, (a_ref, b_ref) in enumerate(((own_a, own_b), (sib_a, sib_b))):
+        @pl.when(pl.program_id(0) == i)
+        def _():
+            q_ref[...] = a_ref[0].T
+            k_ref[...] = a_ref[1].T
+            v_ref[...] = b_ref[0].T
+            o_ref[...] = b_ref[1]
+
+
+def join_attn(core, own, other):
+    _, hid, half_d = own[0].shape
+    block = pl.BlockSpec((2, hid, half_d), lambda i, j, c: (0, 0, 0))
+    tall = pl.BlockSpec((half_d, hid), lambda i, j, c: ((c[0] + i) % 2, 0))
+    wide = pl.BlockSpec((hid, half_d), lambda i, j, c: (0, (c[0] + i) % 2))
+    return join_call(core, join_attn_body, (2, 1), list(own), list(other), [block] * 2, [tall] * 3 + [wide],
+                     [jax.ShapeDtypeStruct((2 * half_d, hid), F32)] * 3 + [jax.ShapeDtypeStruct((hid, 2 * half_d), F32)])
 
 
 def join_flip_body(core_ref, oa_ref, ob_ref, sa_ref, sb_ref, out_ref):
@@ -379,16 +513,10 @@
     return own, [(pp_d(a), pp_d(b)) for a, b in own]
 
 
-def own_terms(tile, first, second):
-    order = (3, first, second, 0)
-    sent = {r: pp_d(tile(r, 1)) for r in order}
-    return {r: tile(r, 0) + sent[r] for r in order}
-
-
 def reduce_terms(total, pp_first, pp_second, first, second):
-    here = total[0] + pp_first(total[first])
-    there = total[second] + pp_first(total[3])
-    return here + pp_second(there)
+    here, there = pp_first(total[first]), pp_first(total[3])
+    last = pp_second(total[second] + there)
+    return total[0] + here + last
 
 
 BOTH = ('model', 'data')
@@ -428,11 +556,6 @@
         def after(v, *deps):
             return lax.optimization_barrier((v,) + deps)[0]
 
-        def keep(hist, v, layer):
-            if hist is None:
-                hist = jnp.zeros((layer_count,) + v.shape, v.dtype)
-            return lax.dynamic_update_slice(hist, v[None], (layer, 0, 0))
-
         def my_tokens(v):
             mine = lax.dynamic_index_in_dim(v, chip_x, 0, keepdims=False)
             half = mine.shape[0] // 2
@@ -456,25 +579,23 @@
         o_all = gather(take(w_o, core, 0, hid // 2))
         w2 = gather_permuted(w_2)
         w1 = gather_permuted(w_1.T)
-        wq, wk, wv = [jnp.concatenate([take(qkv_all, 3 * c + i, 0, hid) for c in chips], axis=0) for i in range(3)]
+        wq = jnp.concatenate([take(qkv_all, 3 * c, 0, hid) for c in chips], axis=0)
+        wkv = jnp.concatenate([take(qkv_all, 3 * c + i, 0, hid) for i in (1, 2) for c in chips], axis=0)
         wo = jnp.concatenate([take(o_all, c, 0, hid) for c in chips], axis=0)
         d_cur = my_tokens(cot_out)
+        emb = step_emb.astype(F32)
 
         saved = []
         g_mine = []
         u_hist = m_hist = ctx_hist = None
         for layer in range(layer_count):
-            s = x_cur.astype(F32) + step_emb[layer].astype(F32)
-            u = rms_norm(s).astype(BF16)
-            kv = jnp.concatenate([nt(u, wk).astype(BF16), nt(u, wv).astype(BF16)], axis=1)
+            e = emb[layer:layer + 1]
+            kv, u_hist = norm_kv(x_cur, e, wkv, layer, layer_count, u_hist)
             kv_s = pp_d(kv)
-            q = nt(u, wq).astype(BF16)
+            q = nt(u_hist[layer], wq).astype(BF16)
             ctx_hist, lse = attn_fwd(q, kv, kv_s, layer, layer_count, ctx_hist)
-            h = (s + nn(ctx_hist[layer], wo)).astype(BF16)
-            z, g, x_next, m_hist = mlp_fwd(h, w1, w2, layer, layer_count, m_hist)
+            z, g, x_next, h, m_hist = mlp_fwd(x_cur, e, ctx_hist, wo, w1, w2, layer, layer_count, m_hist)
             g_mine.append(lax.all_to_all(g.reshape(-1, g.shape[-1]), BOTH, split_axis=0, concat_axis=0, tiled=True))
-            u_hist = keep(u_hist, u, layer)
-            u_hist, x_next = lax.optimization_barrier((u_hist, x_next))
             saved.append((x_cur, q, kv, kv_s, lse, h, z))
             x_cur = x_next
 
@@ -485,43 +606,35 @@
         next_all = [None] * layer_count
         for layer in reversed(range(layer_count)):
             x_l, q, kv, kv_s, lse, h, z = saved[layer]
+            e = emb[layer:layer + 1]
             d_next = d_cur
-            next_all[layer] = gather(d_next)
-            up_hist, mid_hist = mlp_bwd(d_next, h, z, w1, w2, layer, layer_count, up_hist, mid_hist)
-            d_mid = mid_hist[layer]
+            if layer < layer_count - 1:
+                next_all[layer] = gather(d_next)
+            up_hist, mid_hist, d_ctx = mlp_bwd(d_next, h, z, wo, w1, w2, layer, layer_count, up_hist, mid_hist)
             if layer == 0:
                 up_f, m_f = flat(up_hist), flat(m_hist)
-                term_1a, d_mid, up_f = lax.optimization_barrier((tn(up_f, m_f[:, :half_d]), d_mid, up_f))
+                term_1a, d_ctx, up_f = lax.optimization_barrier((tn(up_f, m_f[:, :half_d]), d_ctx, up_f))
                 grad_1a = scatter(term_1a)
                 term_1b = tn(up_f, m_f[:, half_d:])
-                term_1b, d_mid = lax.optimization_barrier((term_1b, d_mid))
+                term_1b, d_ctx = lax.optimization_barrier((term_1b, d_ctx))
                 grad_1b = scatter(term_1b)
-            d_ctx = nt(d_mid, wo).astype(BF16)
-            dq_hist, dko, dks, dvo, dvs = attn_bwd(q, kv, kv_s, d_ctx, lse, layer, layer_count, dq_hist)
-            dk = (dko + pp_d(dks)).astype(BF16)
-            dv = (dvo + pp_d(dvs)).astype(BF16)
-            dk_hist, dv_hist = keep(dk_hist, dk, layer), keep(dv_hist, dv, layer)
-            d_norm1 = (nn(dq_hist[layer], wq) + nn(dk, wk) + nn(dv, wv)).astype(BF16)
-            s = x_l.astype(F32) + step_emb[layer].astype(F32)
-            norm_pull_x = jax.vjp(rms_norm, s)[1]
-            d_cur = (d_mid.astype(F32) + norm_pull_x(d_norm1.astype(F32))[0]).astype(BF16)
-            if layer > 0:
-                d_cur, dk_hist, dv_hist = lax.optimization_barrier((d_cur, dk_hist, dv_hist))
+            dq_hist, own_kv, sib_kv = attn_bwd(q, kv, kv_s, d_ctx, lse, layer, layer_count, dq_hist)
+            recv_kv = pp_d(sib_kv)
+            acc0 = nn(dq_hist[layer], wq)
+            dk_hist, dv_hist, d_cur = d_kv(acc0, x_l, e, mid_hist, own_kv, recv_kv, wkv, layer, layer_count, dk_hist, dv_hist)
 
         mid_half = [lax.optimization_barrier(take(flat(mid_hist), w, 1, half_d)) for w in (core, 1 - core)]
         u_half = [lax.optimization_barrier(take(flat(u_hist), w, 1, half_d)) for w in (core, 1 - core)]
-
-        def cols(v, r):
-            return flat(v)[:, r * hid:(r + 1) * hid]
-
-        t_o = own_terms(lambda r, half: tn(cols(ctx_hist, r), mid_half[half]), 2, 1)
-        t_q = own_terms(lambda r, half: tn(u_half[half], cols(dq_hist, r)), 1, 2)
-        t_k = own_terms(lambda r, half: tn(u_half[half], cols(dk_hist, r)), 1, 2)
-        t_v = own_terms(lambda r, half: tn(u_half[half], cols(dv_hist, r)), 2, 1)
-        own_o = reduce_terms(t_o, pp_y, pp_x, 2, 1)
-        own_q = reduce_terms(t_q, pp_x, pp_y, 1, 2)
-        own_k = reduce_terms(t_k, pp_x, pp_y, 1, 2)
-        own_v = reduce_terms(t_v, pp_y, pp_x, 2, 1)
+        lhs = [flat(v) for v in (dq_hist, dk_hist, dv_hist, ctx_hist)]
+        sent = {}
+        for pair in ((3, 1), (2, 0)):
+            for r, ab in terms(*lhs, u_half[1], mid_half[1], pair, []).items():
+                sent[r] = [pp_d(v) for v in ab]
+        total = {}
+        for pair in ((3, 1), (2, 0)):
+            total.update(terms(*lhs, u_half[0], mid_half[0], pair, sent[pair[0]] + sent[pair[1]]))
+        own_qk = reduce_terms({r: v[0] for r, v in total.items()}, pp_x, pp_y, 1, 2)
+        own_vo = reduce_terms({r: v[1] for r, v in total.items()}, pp_y, pp_x, 2, 1)
 
         def ordered(own, sib, axis):
             size = own.shape[axis]
@@ -537,16 +650,21 @@
         d_x = jnp.zeros((2,) + whole.shape, BF16)
         d_x = put(put(d_x, row_seq[None], chip_x, 0), from_x[None], 1 - chip_x, 0)
 
-        ready = tuple(t[r] for t in (t_o, t_q, t_k, t_v) for r in (1, 2, 3))
+        ready = tuple(v for ab in total.values() for v in ab)
+        cot_mine = cot_out.reshape(-1, dim)
+        cot_other = pp_d(cot_mine)
         grad_2 = None
         for layer in reversed(range(layer_count)):
-            term = tn(after(g_mine[layer], *ready), next_all[layer])
-            grad_2 = term if grad_2 is None else grad_2 + term
-
-        (grad_2,) = join(core, [grad_2], [pp_d(grad_2)], (0,), 4)
+            g_all = after(g_mine[layer], *ready)
+            if layer == layer_count - 1:
+                rows = g_all.shape[0] // 2
+                grad_2 = tn(take(g_all, core, 0, rows), cot_mine) + tn(take(g_all, 1 - core, 0, rows), cot_other)
+            else:
+                grad_2 = grad_2 + tn(g_all, next_all[layer])
+
+        grad_2 = join(core, grad_2, pp_d(grad_2))
         grad_1 = join_flip(core, [grad_1a, grad_1b], [pp_d(grad_1a), pp_d(grad_1b)])
-        own = [own_q, own_k, own_v, own_o]
-        gq, gk, gv, go = join(core, own, [pp_d(v) for v in own], (0, 0, 0, 1), 1)
+        gq, gk, gv, go = join_attn(core, (own_qk, own_vo), (pp_d(own_qk), pp_d(own_vo)))
         return gq, gk, gv, go, grad_1, grad_2, d_x
 
     return jax.shard_map(device_step, mesh=mesh,

time: 1870 us -> 1760 us (0.941)
  Pallas kernels: 538 us -> 781 us
  matrix products: 385 us -> 179 us
  waiting for transfers between devices: 644 us -> 566 us
  other arithmetic: 65.1 us -> 31.8 us
    pallas_call x4 -> x16, Pallas kernels: 126 us -> 351 us  [the longest x4 147 us: mlp_bwd(): pl.pallas_call(mlp_bwd_body, grid=(hidden // BLOCK_B,), in_specs=[whole,...]
    dot_general x70 -> x15, matrix products: 385 us -> 179 us  [dot(): return lax.dot_general(a, b, (dims, ((), ())), preferred_element_type=F32)]
    ppermute x12 -> x9, waiting for transfers between devices: 237 us -> 161 us  [pp_y(): return lax.ppermute(v, 'model', SWAP_Y)]
    ppermute x13 -> x10, waiting for transfers between devices: 243 us -> 178 us  [pp_x(): return lax.ppermute(v, 'model', SWAP_X)]
    all_to_all x4, waiting for transfers between devices: 143 us -> 206 us  [device_step(): lax.all_to_all(g.reshape(-1, g.shape[-1]), BOTH, split_axis=0, concat_axi...]
    dynamic_update_slice x9 -> x0, other arithmetic: 21.4 us -> none  [keep(): return lax.dynamic_update_slice(hist, v[None], (layer, 0, 0))]
    dynamic_update_slice x28 -> x29, local copies, waits for them, and re-layouts: 54.7 us -> 52.1 us  [put(): return lax.dynamic_update_slice_in_dim(buf, v, which * v.shape[axis], axis)]
  transfers between devices with their start and end apart: 88 -> 68, of which waited for: 23 -> 22; matrix products, arithmetic and copies ran while one was open for 30% -> 19% of each run, Pallas kernels for 26% -> 24%
where the time goes in v6:
time: 1760 us
  Pallas kernels  781 us (44%)
  waiting for transfers between devices  566 us (32%)
  matrix products  179 us (10%)
  local copies, waits for them, and re-layouts  131 us (7%)
  starting transfers between devices  54.8 us (3%)
  other arithmetic  31.8 us (2%)
    all_to_all x4, waiting for transfers between devices, device_step(): lax.all_to_all(g.reshape(-1, g.shape[-1]), BOTH, split_axis=0, concat_axi...  206 us
    dot_general x15, matrix products, dot(): return lax.dot_general(a, b, (dims, ((), ())), preferred_element_type=F32)  179 us
    ppermute x10, waiting for transfers between devices, pp_x(): return lax.ppermute(v, 'model', SWAP_X)  178 us
    pallas_call x4, Pallas kernels, attn_bwd(): pl.pallas_call(attn_bwd_body, grid=(pairs,), in_specs=[pl.BlockSpec((tq,...  173 us
    ppermute x9, waiting for transfers between devices, pp_y(): return lax.ppermute(v, 'model', SWAP_Y)  161 us
    pallas_call x4, Pallas kernels, mlp_bwd(): pl.pallas_call(mlp_bwd_body, grid=(hidden // BLOCK_B,), in_specs=[whole,...  147 us
    pallas_call x4, Pallas kernels, mlp_fwd(): pl.pallas_call(mlp_fwd_body, grid=(hidden // BLOCK_F,), in_specs=[whole,...  134 us
    pallas_call x4, Pallas kernels, attn_fwd(): pl.pallas_call(attn_fwd_body, grid=(pairs,), in_specs=[pl.BlockSpec((tq,...  94.3 us
  transfers between devices with their start and end apart: 68, of which 22 were waited for; matrix products, arithmetic and copies ran while one was open for 19% of the time, Pallas kernels for 24%

profile of v6, /device:TPU:0, one launch (start us, length us, event | category | flops | bytes accessed | tf_op | source)
XLA Modules:
  0.0 1759.1 jit_solution(14104096992508590149)
XLA Ops:
  16.2 6.6 copy.43
  39.5 7.3 broadcast.6.clone
  50.0 26.7 %collective-permute-done.2 = bf16[384,1536]{1,0:T(8,128)(2,1)} collective-permute-done((bf16[384,1536]{1,0:T(8,128)(2,1)}, bf16[384,1536]{1,0:T(8,128)(2,1)}, u32[]{:S(2)}, u32[]{:S(2)}) %collective-permute-start.2) | collective-permute-done | bytes 1179680 | tf_op jit(solution)/shard_map/ppermute | solution.py:27
  77.1 6.6 broadcast.6.clone.1
  86.1 41.1 %collective-permute-done.4 = bf16[384,1536]{1,0:T(8,128)(2,1)} collective-permute-done((bf16[384,1536]{1,0:T(8,128)(2,1)}, bf16[384,1536]{1,0:T(8,128)(2,1)}, u32[]{:S(2)}, u32[]{:S(2)}) %collective-permute-start.4) | collective-permute-done | bytes 1179680 | tf_op jit(solution)/shard_map/ppermute | solution.py:27
  131.7 34.3 %collective-permute-done.14 = bf16[384,1536]{1,0:T(8,128)(2,1)} collective-permute-done((bf16[384,1536]{1,0:T(8,128)(2,1)}, bf16[384,1536]{1,0:T(8,128)(2,1)}, u32[]{:S(2)}, u32[]{:S(2)}) %collective-permute-start.14) | collective-permute-done | bytes 1179680 | tf_op jit(solution)/shard_map/ppermute | solution.py:27
  175.4 29.8 %collective-permute-done.16 = bf16[384,1536]{1,0:T(8,128)(2,1)S(1)} collective-permute-done((bf16[384,1536]{1,0:T(8,128)(2,1)S(1)}, bf16[384,1536]{1,0:T(8,128)(2,1)S(1)}, u32[]{:S(2)}, u32[]{:S(2)}) %collective-permute-start.16) | collective-permute-done | bytes 1179680 | tf_op jit(solution)/shard_map/ppermute | solution.py:27
  217.1 19.5 %collective-permute-done.20 = bf16[384,1536]{1,0:T(8,128)(2,1)S(1)} collective-permute-done((bf16[384,1536]{1,0:T(8,128)(2,1)S(1)}, bf16[384,1536]{1,0:T(8,128)(2,1)S(1)}, u32[]{:S(2)}, u32[]{:S(2)}) %collective-permute-start.20) | collective-permute-done | bytes 1179680 | tf_op jit(solution)/shard_map/ppermute | solution.py:31
  244.6 17.3 collective-permute-done.10
  265.4 21.2 %collective-permute-done.22 = bf16[384,1536]{1,0:T(8,128)(2,1)} collective-permute-done((bf16[384,1536]{1,0:T(8,128)(2,1)}, bf16[384,1536]{1,0:T(8,128)(2,1)}, u32[]{:S(2)}, u32[]{:S(2)}) %collective-permute-start.22) | collective-permute-done | bytes 1179680 | tf_op jit(solution)/shard_map/ppermute | solution.py:31
  313.4 10.8 norm_kv.4
  340.9 7.7 convolution_convert_fusion.3.refs_0_.refs_1_
  348.5 23.6 %attn_fwd.4 = (bf16[4,512,1536]{2,1,0:T(8,128)(2,1)}, f32[12,2,512]{2,1,0:T(2,128)}) custom-call(bf16[512,1536]{1,0:T(8,128)(2,1)} %convolution_convert_fusion.3.refs_0_.refs_1_, bf16[512,1536]{1,0:T(8,128)(2,1)} %convolution_convert_fusion.3.refs_0_.refs_1_, bf16[512,3072]{1,0:T(8,128)(2,1)} %get-tuple-element.108.refs_2_.refs_4_.refs_6_.refs_1_.refs_3_, ...), custom_call_target="tpu_custom_call" | custom-call | flops 12884901888 | bytes 9437184 | tf_op jit(solution)/shard_map/attn_fwd/pallas_call | solution.py:114
  372.1 33.6 %mlp_fwd.4 = (bf16[512,6144]{1,0:T(8,128)(2,1)}, bf16[8,512,768]{2,1,0:T(8,128)(2,1)}, bf16[512,1536]{1,0:T(8,128)(2,1)}, bf16[512,1536]{1,0:T(8,128)(2,1)}, bf16[4,512,1536]{2,1,0:T(8,128)(2,1)}) custom-call(bf16[512,1536]{1,0:T(8,128)(2,1)} %bitcast_select_fusion.1.refs_0_.refs_1_, f32[1,1536]{1,0:T(1,128)} %get-tuple-element.229.refs_1_.refs_2_, ...), custom_call_target="tpu_custom_call" | custom-call | flops 19327352832 | bytes 50331648 | tf_op jit(solution)/shard_map/mlp_fwd/pallas_call | solution.py:365
  405.8 10.0 norm_kv.5
  421.8 23.8 %attn_fwd.5 = (bf16[4,512,1536]{2,1,0:T(8,128)(2,1)}, f32[12,2,512]{2,1,0:T(2,128)}) custom-call(bf16[512,1536]{1,0:T(8,128)(2,1)} %convolution_convert_fusion.2.refs_0_.refs_1_, bf16[512,1536]{1,0:T(8,128)(2,1)} %convolution_convert_fusion.2.refs_0_.refs_1_, ...), custom_call_target="tpu_custom_call", output_to_operand_aliasing={{0}: (8, {})} | custom-call | flops 12884901888 | bytes 9437184 | tf_op jit(solution)/shard_map/attn_fwd/pallas_call | solution.py:114
  445.7 33.5 %mlp_fwd.5 = (bf16[512,6144]{1,0:T(8,128)(2,1)}, bf16[8,512,768]{2,1,0:T(8,128)(2,1)}, bf16[512,1536]{1,0:T(8,128)(2,1)}, bf16[512,1536]{1,0:T(8,128)(2,1)}, bf16[4,512,1536]{2,1,0:T(8,128)(2,1)}) custom-call(bf16[512,1536]{1,0:T(8,128)(2,1)} %get-tuple-element.110.refs_0_.refs_1_, ...), custom_call_target="tpu_custom_call", output_to_operand_aliasing={{4}: (6, {})} | custom-call | flops 19327352832 | bytes 50331648 | tf_op jit(solution)/shard_map/mlp_fwd/pallas_call | solution.py:365
  479.2 9.9 norm_kv.6
  495.1 23.5 %attn_fwd.6 = (bf16[4,512,1536]{2,1,0:T(8,128)(2,1)}, f32[12,2,512]{2,1,0:T(2,128)}) custom-call(bf16[512,1536]{1,0:T(8,128)(2,1)} %convolution_convert_fusion.1.refs_0_.refs_1_, bf16[512,1536]{1,0:T(8,128)(2,1)} %convolution_convert_fusion.1.refs_0_.refs_1_, ...), custom_call_target="tpu_custom_call", output_to_operand_aliasing={{0}: (8, {})} | custom-call | flops 12884901888 | bytes 9437184 | tf_op jit(solution)/shard_map/attn_fwd/pallas_call | solution.py:114
  518.6 33.7 %mlp_fwd.6 = (bf16[512,6144]{1,0:T(8,128)(2,1)}, bf16[8,512,768]{2,1,0:T(8,128)(2,1)}, bf16[512,1536]{1,0:T(8,128)(2,1)}, bf16[512,1536]{1,0:T(8,128)(2,1)}, bf16[4,512,1536]{2,1,0:T(8,128)(2,1)}) custom-call(bf16[512,1536]{1,0:T(8,128)(2,1)} %get-tuple-element.115.refs_0_.refs_1_, ...), custom_call_target="tpu_custom_call", output_to_operand_aliasing={{4}: (6, {})} | custom-call | flops 19327352832 | bytes 50331648 | tf_op jit(solution)/shard_map/mlp_fwd/pallas_call | solution.py:365
  552.3 10.0 norm_kv.7
  564.6 5.8 collective-permute-done.29
  573.5 7.7 convolution_convert_fusion.refs_0_.refs_1_
  581.2 23.4 %attn_fwd.7 = (bf16[4,512,1536]{2,1,0:T(8,128)(2,1)}, f32[12,2,512]{2,1,0:T(2,128)}) custom-call(bf16[512,1536]{1,0:T(8,128)(2,1)} %convolution_convert_fusion.refs_0_.refs_1_, bf16[512,1536]{1,0:T(8,128)(2,1)} %convolution_convert_fusion.refs_0_.refs_1_, ...), custom_call_target="tpu_custom_call", output_to_operand_aliasing={{0}: (8, {})} | custom-call | flops 12884901888 | bytes 9437184 | tf_op jit(solution)/shard_map/attn_fwd/pallas_call | solution.py:114
  604.6 33.6 %mlp_fwd.7 = (bf16[512,6144]{1,0:T(8,128)(2,1)}, bf16[8,512,768]{2,1,0:T(8,128)(2,1)}, bf16[512,1536]{1,0:T(8,128)(2,1)}, bf16[512,1536]{1,0:T(8,128)(2,1)}, bf16[4,512,1536]{2,1,0:T(8,128)(2,1)}) custom-call(bf16[512,1536]{1,0:T(8,128)(2,1)} %get-tuple-element.120.refs_0_.refs_1_, ...), custom_call_target="tpu_custom_call", output_to_operand_aliasing={{4}: (6, {})} | custom-call | flops 19327352832 | bytes 50331648 | tf_op jit(solution)/shard_map/mlp_fwd/pallas_call | solution.py:365
  638.2 36.3 %mlp_bwd.4 = (bf16[4,512,6144]{2,1,0:T(8,128)(2,1)}, bf16[4,512,1536]{2,1,0:T(8,128)(2,1)}, bf16[512,1536]{1,0:T(8,128)(2,1)}) custom-call(bf16[512,1536]{1,0:T(8,128)(2,1)} %bitcast_select_fusion.refs_0_, bf16[512,1536]{1,0:T(8,128)(2,1)} %get-tuple-element.125.refs_1_, bf16[512,6144]{1,0:T(8,128)(2,1)} %get-tuple-element.126.refs_2_, ...), custom_call_target="tpu_custom_call" | custom-call | flops 19327352832 | bytes 50331648 | tf_op jit(solution)/shard_map/mlp_bwd/pallas_call | solution.py:428
  674.5 43.2 %attn_bwd.4 = (bf16[4,512,1536]{2,1,0:T(8,128)(2,1)}, f32[2,512,1536]{2,1,0:T(8,128)}, f32[2,512,1536]{2,1,0:T(8,128)}) custom-call(bf16[512,1536]{1,0:T(8,128)(2,1)} %convolution_convert_fusion.refs_0_.refs_1_, bf16[512,3072]{1,0:T(8,128)(2,1)} %get-tuple-element.122.refs_2_.refs_4_.refs_6_.refs_1_.refs_3_, ...), custom_call_target="tpu_custom_call" | custom-call | flops 32212254720 | bytes 25165824 | tf_op jit(solution)/shard_map/attn_bwd/pallas_call | solution.py:182
  717.8 6.2 fusion.17.refs_0_
  728.1 16.6 d_kv.4
  744.8 37.1 %mlp_bwd.5 = (bf16[4,512,6144]{2,1,0:T(8,128)(2,1)}, bf16[4,512,1536]{2,1,0:T(8,128)(2,1)}, bf16[512,1536]{1,0:T(8,128)(2,1)}) custom-call(bf16[512,1536]{1,0:T(8,128)(2,1)} %get-tuple-element.133.refs_0_, bf16[512,1536]{1,0:T(8,128)(2,1)} %get-tuple-element.134.refs_1_, ...), custom_call_target="tpu_custom_call", output_to_operand_aliasing={{0}: (6, {}), {1}: (7, {})} | custom-call | flops 19327352832 | bytes 50331648 | tf_op jit(solution)/shard_map/mlp_bwd/pallas_call | solution.py:428
  782.0 43.2 %attn_bwd.5 = (bf16[4,512,1536]{2,1,0:T(8,128)(2,1)}, f32[2,512,1536]{2,1,0:T(8,128)}, f32[2,512,1536]{2,1,0:T(8,128)}) custom-call(bf16[512,1536]{1,0:T(8,128)(2,1)} %convolution_convert_fusion.1.refs_0_.refs_1_, bf16[512,3072]{1,0:T(8,128)(2,1)} %get-tuple-element.117.refs_2_.refs_4_.refs_6_.refs_1_.refs_3_, ...), custom_call_target="tpu_custom_call", output_to_operand_aliasing={{0}: (7, {})} | custom-call | flops 32212254720 | bytes 25165824 | tf_op jit(solution)/shard_map/attn_bwd/pallas_call | solution.py:182
  825.2 6.0 fusion.15.refs_0_
  835.6 17.2 d_kv.5
  852.9 36.9 %mlp_bwd.6 = (bf16[4,512,6144]{2,1,0:T(8,128)(2,1)}, bf16[4,512,1536]{2,1,0:T(8,128)(2,1)}, bf16[512,1536]{1,0:T(8,128)(2,1)}) custom-call(bf16[512,1536]{1,0:T(8,128)(2,1)} %get-tuple-element.145.refs_0_, bf16[512,1536]{1,0:T(8,128)(2,1)} %get-tuple-element.146.refs_1_, ...), custom_call_target="tpu_custom_call", output_to_operand_aliasing={{0}: (6, {}), {1}: (7, {})} | custom-call | flops 19327352832 | bytes 50331648 | tf_op jit(solution)/shard_map/mlp_bwd/pallas_call | solution.py:428
  889.8 43.2 %attn_bwd.6 = (bf16[4,512,1536]{2,1,0:T(8,128)(2,1)}, f32[2,512,1536]{2,1,0:T(8,128)}, f32[2,512,1536]{2,1,0:T(8,128)}) custom-call(bf16[512,1536]{1,0:T(8,128)(2,1)} %convolution_convert_fusion.2.refs_0_.refs_1_, bf16[512,3072]{1,0:T(8,128)(2,1)} %get-tuple-element.112.refs_2_.refs_4_.refs_6_.refs_1_.refs_3_, ...), custom_call_target="tpu_custom_call", output_to_operand_aliasing={{0}: (7, {})} | custom-call | flops 32212254720 | bytes 25165824 | tf_op jit(solution)/shard_map/attn_bwd/pallas_call | solution.py:182
  933.1 6.0 fusion.13.refs_0_
  943.5 16.8 d_kv.6
  960.4 36.9 %mlp_bwd.7 = (bf16[4,512,6144]{2,1,0:T(8,128)(2,1)}, bf16[4,512,1536]{2,1,0:T(8,128)(2,1)}, bf16[512,1536]{1,0:T(8,128)(2,1)}) custom-call(bf16[512,1536]{1,0:T(8,128)(2,1)} %get-tuple-element.157.refs_0_, bf16[512,1536]{1,0:T(8,128)(2,1)} %get-tuple-element.158.refs_1_, ...), custom_call_target="tpu_custom_call", output_to_operand_aliasing={{0}: (6, {}), {1}: (7, {})} | custom-call | flops 19327352832 | bytes 50331648 | tf_op jit(solution)/shard_map/mlp_bwd/pallas_call | solution.py:428
  997.3 26.4 %fusion.2 = f32[6144,768]{1,0:T(8,128)} fusion(bf16[2048,6144]{1,0:T(8,128)(2,1)} %bitcast.67, bf16[2048,1536]{1,0:T(8,128)(2,1)} %bitcast.92), kind=kOutput, calls=%fused_computation.9 | convolution fusion | flops 19327352832 | bytes 47185920 | tf_op jit(solution)/shard_map/dot_general | solution.py:39
  1023.7 27.0 %fusion = f32[6144,768]{1,0:T(8,128)} fusion(bf16[2048,6144]{1,0:T(8,128)(2,1)} %bitcast.68, bf16[2048,1536]{1,0:T(8,128)(2,1)} %bitcast.93), kind=kOutput, calls=%fused_computation.7 | convolution fusion | flops 19327352832 | bytes 47185920 | tf_op jit(solution)/shard_map/dot_general | solution.py:39
  1055.0 110.2 %all-to-all-done.3 = bf16[8,512,768]{2,1,0:T(8,128)(2,1)} async-done(((bf16[8,512,768]{2,1,0:T(8,128)(2,1)}), bf16[8,512,768]{2,1,0:T(8,128)(2,1)}, u32[]{:S(2)}, u32[]{:S(2)}) %all-to-all-start.3) | async-done | bytes 6291488 | tf_op jit(solution)/shard_map/all_to_all | solution.py:598
  1168.7 43.3 %attn_bwd.7 = (bf16[4,512,1536]{2,1,0:T(8,128)(2,1)}, f32[2,512,1536]{2,1,0:T(8,128)}, f32[2,512,1536]{2,1,0:T(8,128)}) custom-call(bf16[512,1536]{1,0:T(8,128)(2,1)} %convolution_convert_fusion.3.refs_0_.refs_1_, bf16[512,3072]{1,0:T(8,128)(2,1)} %get-tuple-element.108.refs_2_.refs_4_.refs_6_.refs_1_.refs_3_, ...), custom_call_target="tpu_custom_call", output_to_operand_aliasing={{0}: (7, {})} | custom-call | flops 32212254720 | bytes 25165824 | tf_op jit(solution)/shard_map/attn_bwd/pallas_call | solution.py:182
  1212.3 6.0 constant_dynamic-slice_fusion.1
  1218.3 50.7 %all-to-all-done.1 = bf16[8,512,768]{2,1,0:T(8,128)(2,1)} async-done(((bf16[8,512,768]{2,1,0:T(8,128)(2,1)}), bf16[8,512,768]{2,1,0:T(8,128)(2,1)}, u32[]{:S(2)}, u32[]{:S(2)}) %all-to-all-start.1) | async-done | bytes 6291488 | tf_op jit(solution)/shard_map/all_to_all | solution.py:598
  1273.1 7.5 constant_dynamic-slice_fusion
  1280.6 5.7 fusion.11.refs_0_
  1286.3 20.5 %d_kv.7 = (bf16[4,512,1536]{2,1,0:T(8,128)(2,1)}, bf16[4,512,1536]{2,1,0:T(8,128)(2,1)}, bf16[512,1536]{1,0:T(8,128)(2,1)}) custom-call(f32[512,1536]{1,0:T(8,128)} %fusion.11.refs_0_, bf16[512,1536]{1,0:T(8,128)(2,1)} %bitcast_select_fusion.1.refs_0_.refs_1_, ...), custom_call_target="tpu_custom_call", output_to_operand_aliasing={{0}: (7, {}), {1}: (8, {})} | custom-call | flops 4831838208 | bytes 25165824 | tf_op jit(solution)/shard_map/d_kv/pallas_call | solution.py:272
  1307.2 21.8 %shard_map.146 = (f32[2,384,768]{2,1,0:T(8,128)}, f32[2,384,768]{2,1,0:T(8,128)}, f32[2,384,768]{2,1,0:T(8,128)}, f32[2,384,768]{2,1,0:T(8,128)}) custom-call(bf16[2048,1536]{1,0:T(8,128)(2,1)} %bitcast.79, bf16[2048,1536]{1,0:T(8,128)(2,1)} %bitcast.69, bf16[2048,1536]{1,0:T(8,128)(2,1)} %bitcast.73, bf16[2048,1536]{1,0:T(8,128)(2,1)} %bitcast.83, ...), custom_call_target="tpu_custom_call" | custom-call | flops 9663676416 | bytes 18874368 | tf_op jit(solution)/shard_map/pallas_call | solution.py:310
  1330.1 21.9 %shard_map.144 = (f32[2,384,768]{2,1,0:T(8,128)}, f32[2,384,768]{2,1,0:T(8,128)}, f32[2,384,768]{2,1,0:T(8,128)}, f32[2,384,768]{2,1,0:T(8,128)}) custom-call(bf16[2048,1536]{1,0:T(8,128)(2,1)} %bitcast.80, bf16[2048,1536]{1,0:T(8,128)(2,1)} %bitcast.70, bf16[2048,1536]{1,0:T(8,128)(2,1)} %bitcast.74, bf16[2048,1536]{1,0:T(8,128)(2,1)} %bitcast.84, ...), custom_call_target="tpu_custom_call" | custom-call | flops 9663676416 | bytes 18874368 | tf_op jit(solution)/shard_map/pallas_call | solution.py:310
  1354.5 26.2 %all-to-all-done = bf16[8,512,768]{2,1,0:T(8,128)(2,1)} async-done(((bf16[8,512,768]{2,1,0:T(8,128)(2,1)}), bf16[8,512,768]{2,1,0:T(8,128)(2,1)}, u32[]{:S(2)}, u32[]{:S(2)}) %all-to-all-start) | async-done | bytes 6291488 | tf_op jit(solution)/shard_map/all_to_all | solution.py:598
  1391.4 23.4 %shard_map.147 = (f32[2,384,768]{2,1,0:T(8,128)}, f32[2,384,768]{2,1,0:T(8,128)}, f32[2,384,768]{2,1,0:T(8,128)}, f32[2,384,768]{2,1,0:T(8,128)}) custom-call(bf16[2048,1536]{1,0:T(8,128)(2,1)} %bitcast.81, bf16[2048,1536]{1,0:T(8,128)(2,1)} %bitcast.71, bf16[2048,1536]{1,0:T(8,128)(2,1)} %bitcast.75, bf16[2048,1536]{1,0:T(8,128)(2,1)} %bitcast.85, ...), custom_call_target="tpu_custom_call" | custom-call | flops 9663676416 | bytes 18874368 | tf_op jit(solution)/shard_map/pallas_call | solution.py:310
  1420.4 24.4 %shard_map.145 = (f32[2,384,768]{2,1,0:T(8,128)}, f32[2,384,768]{2,1,0:T(8,128)}, f32[2,384,768]{2,1,0:T(8,128)}, f32[2,384,768]{2,1,0:T(8,128)}) custom-call(bf16[2048,1536]{1,0:T(8,128)(2,1)} %bitcast.82, bf16[2048,1536]{1,0:T(8,128)(2,1)} %bitcast.72, bf16[2048,1536]{1,0:T(8,128)(2,1)} %bitcast.76, bf16[2048,1536]{1,0:T(8,128)(2,1)} %bitcast.86, ...), custom_call_target="tpu_custom_call" | custom-call | flops 9663676416 | bytes 18874368 | tf_op jit(solution)/shard_map/pallas_call | solution.py:310
  1448.1 10.3 fusion.6
  1459.1 10.0 fusion.4
  1469.1 19.0 %all-to-all-done.2 = bf16[8,512,768]{2,1,0:T(8,128)(2,1)} async-done(((bf16[8,512,768]{2,1,0:T(8,128)(2,1)}), bf16[8,512,768]{2,1,0:T(8,128)(2,1)}, u32[]{:S(2)}, u32[]{:S(2)}) %all-to-all-start.2) | async-done | bytes 6291488 | tf_op jit(solution)/shard_map/all_to_all | solution.py:598
  1488.1 17.0 fusion.35
  1505.1 89.3 %collective-permute-done.46 = f32[2,384,768]{2,1,0:T(8,128)} collective-permute-done((f32[2,384,768]{2,1,0:T(8,128)}, f32[2,384,768]{2,1,0:T(8,128)}, u32[]{:S(2)}, u32[]{:S(2)}) %collective-permute-start.46) | collective-permute-done | bytes 2359328 | tf_op jit(solution)/shard_map/ppermute | solution.py:31
  1614.2 16.3 fusion.36
  1630.5 21.9 %add_add_fusion.refs_0_ = f32[768,1536]{1,0:T(8,128)} fusion(f32[768,1536]{1,0:T(8,128)} %fusion.36, f32[768,1536]{1,0:T(8,128)} %fusion.35, f32[768,1536]{1,0:T(8,128)} %fusion.6, f32[768,1536]{1,0:T(8,128)} %fusion.4, bf16[4096,768]{1,0:T(8,128)(2,1)} %bitcast.28, bf16[4096,1536]{1,0:T(8,128)(2,1)} %all-gather.14.cloned.1.call-done), kind=kOutput, calls=%fused_computation.3 | convolution fusion | flops 9668395008 | bytes 42467328 | tf_op jit(solution)/shard_map/dot_general | solution.py:39
  1656.1 14.0 collective-permute-done.44
  1676.6 42.0 %collective-permute-done.56 = bf16[1024,1536]{1,0:T(8,128)(2,1)} collective-permute-done((bf16[1024,1536]{1,0:T(8,128)(2,1)}, bf16[1024,1536]{1,0:T(8,128)(2,1)}, u32[]{:S(2)}, u32[]{:S(2)}) %collective-permute-start.56) | collective-permute-done | bytes 3145760 | tf_op jit(solution)/shard_map/ppermute | solution.py:27
  1723.2 8.5 shard_map.148
  1731.7 11.5 shard_map.150
  1743.2 8.8 shard_map.149
  (243 shorter events, 214.3 us)
Async XLA Ops:
  7.2 288.2 %all-gather.6.cloned.1.call-start = ((), (), s32[]{:S(2)}) async-start(), calls=%async_computation.6 | async-start | bytes 15925248 | tf_op jit(solution)/shard_map/all_gather | solution.py:551
  16.1 319.3 %all-gather.8.cloned.1.call-start = ((), (), s32[]{:S(2)}) async-start(), calls=%async_computation.7 | async-start | bytes 5308416 | tf_op jit(solution)/shard_map/all_gather | solution.py:551
  26.5 50.1 %collective-permute-start.2 = (bf16[384,1536]{1,0:T(8,128)(2,1)}, bf16[384,1536]{1,0:T(8,128)(2,1)}, u32[]{:S(2)}, u32[]{:S(2)}) collective-permute-start(bf16[384,1536]{1,0:T(8,128)(2,1)} %get-tuple-element.225), channel_id=1, source_target_pairs={{0,2},{2,0},{4,6},{6,4},{1,3},{3,1},{5,7},{7,5}} | collective-permute-start | bytes 3538952 | tf_op jit(solution)/shard_map/ppermute | solution.py:27
  29.9 100.3 %collective-permute-start.6 = (bf16[384,1536]{1,0:T(8,128)(2,1)}, bf16[384,1536]{1,0:T(8,128)(2,1)}, u32[]{:S(2)}, u32[]{:S(2)}) collective-permute-start(bf16[384,1536]{1,0:T(8,128)(2,1)} %get-tuple-element.225), channel_id=1, source_target_pairs={{0,4},{4,0},{2,6},{6,2},{1,5},{5,1},{3,7},{7,3}} | collective-permute-start | bytes 3538952 | tf_op jit(solution)/shard_map/ppermute | solution.py:31
  31.4 95.8 %collective-permute-start.4 = (bf16[384,1536]{1,0:T(8,128)(2,1)}, bf16[384,1536]{1,0:T(8,128)(2,1)}, u32[]{:S(2)}, u32[]{:S(2)}) collective-permute-start(bf16[384,1536]{1,0:T(8,128)(2,1)} %get-tuple-element.224), channel_id=1, source_target_pairs={{0,2},{2,0},{4,6},{6,4},{1,3},{3,1},{5,7},{7,5}} | collective-permute-start | bytes 3538952 | tf_op jit(solution)/shard_map/ppermute | solution.py:27
  35.1 131.0 %collective-permute-start.14 = (bf16[384,1536]{1,0:T(8,128)(2,1)}, bf16[384,1536]{1,0:T(8,128)(2,1)}, u32[]{:S(2)}, u32[]{:S(2)}) collective-permute-start(bf16[384,1536]{1,0:T(8,128)(2,1)} %get-tuple-element.219), channel_id=1, source_target_pairs={{0,2},{2,0},{4,6},{6,4},{1,3},{3,1},{5,7},{7,5}} | collective-permute-start | bytes 3538952 | tf_op jit(solution)/shard_map/ppermute | solution.py:27
  38.3 129.3 %collective-permute-start = (bf16[512,1536]{1,0:T(8,128)(2,1)S(1)}, bf16[512,1536]{1,0:T(8,128)(2,1)}, u32[]{:S(2)}, u32[]{:S(2)}) collective-permute-start(bf16[512,1536]{1,0:T(8,128)(2,1)S(1)} %dynamic-slice_bitcast_fusion.2), channel_id=1, source_target_pairs={{0,1},{1,0},{2,3},{3,2},{4,5},{5,4},{6,7},{7,6}} | collective-permute-start | bytes 4718600 | tf_op jit(solution)/shard_map/ppermute | solution.py:35
  39.3 1448.8 %all-gather.10.cloned.1.call-start = ((), (), s32[]{:S(2)}) async-start(), calls=%async_computation.10 | async-start | bytes 14155776 | tf_op jit(solution)/shard_map/all_gather | solution.py:551
  76.6 93.5 %collective-permute-start.3 = (bf16[384,1536]{1,0:T(8,128)(2,1)}, bf16[384,1536]{1,0:T(8,128)(2,1)S(1)}, u32[]{:S(2)}, u32[]{:S(2)}) collective-permute-start(bf16[384,1536]{1,0:T(8,128)(2,1)} %collective-permute-done.2), channel_id=1, source_target_pairs={{0,1},{1,0},{2,3},{3,2},{4,5},{5,4},{6,7},{7,6}} | collective-permute-start | bytes 3538952 | tf_op jit(solution)/shard_map/ppermute | solution.py:35
  127.2 78.0 %collective-permute-start.16 = (bf16[384,1536]{1,0:T(8,128)(2,1)S(1)}, bf16[384,1536]{1,0:T(8,128)(2,1)S(1)}, u32[]{:S(2)}, u32[]{:S(2)}) collective-permute-start(bf16[384,1536]{1,0:T(8,128)(2,1)S(1)} %copy-done.20), channel_id=1, source_target_pairs={{0,2},{2,0},{4,6},{6,4},{1,3},{3,1},{5,7},{7,5}} | collective-permute-start | bytes 3538952 | tf_op jit(solution)/shard_map/ppermute | solution.py:27
  130.1 77.6 %collective-permute-start.8 = (bf16[384,1536]{1,0:T(8,128)(2,1)}, bf16[384,1536]{1,0:T(8,128)(2,1)S(1)}, u32[]{:S(2)}, u32[]{:S(2)}) collective-permute-start(bf16[384,1536]{1,0:T(8,128)(2,1)} %get-tuple-element.224), channel_id=1, source_target_pairs={{0,4},{4,0},{2,6},{6,2},{1,5},{5,1},{3,7},{7,3}} | collective-permute-start | bytes 3538952 | tf_op jit(solution)/shard_map/ppermute | solution.py:31
  166.1 43.2 %collective-permute-start.18 = (bf16[384,1536]{1,0:T(8,128)(2,1)}, bf16[384,1536]{1,0:T(8,128)(2,1)S(1)}, u32[]{:S(2)}, u32[]{:S(2)}) collective-permute-start(bf16[384,1536]{1,0:T(8,128)(2,1)} %get-tuple-element.219), channel_id=1, source_target_pairs={{0,4},{4,0},{2,6},{6,2},{1,5},{5,1},{3,7},{7,3}} | collective-permute-start | bytes 3538952 | tf_op jit(solution)/shard_map/ppermute | solution.py:31
  167.7 41.7 %collective-permute-start.15 = (bf16[384,1536]{1,0:T(8,128)(2,1)}, bf16[384,1536]{1,0:T(8,128)(2,1)S(1)}, u32[]{:S(2)}, u32[]{:S(2)}) collective-permute-start(bf16[384,1536]{1,0:T(8,128)(2,1)} %collective-permute-done.14), channel_id=1, source_target_pairs={{0,1},{1,0},{2,3},{3,2},{4,5},{5,4},{6,7},{7,6}} | collective-permute-start | bytes 3538952 | tf_op jit(solution)/shard_map/ppermute | solution.py:35
  170.1 42.0 %collective-permute-start.5 = (bf16[384,1536]{1,0:T(8,128)(2,1)}, bf16[384,1536]{1,0:T(8,128)(2,1)S(1)}, u32[]{:S(2)}, u32[]{:S(2)}) collective-permute-start(bf16[384,1536]{1,0:T(8,128)(2,1)} %collective-permute-done.4), channel_id=1, source_target_pairs={{0,1},{1,0},{2,3},{3,2},{4,5},{5,4},{6,7},{7,6}} | collective-permute-start | bytes 3538952 | tf_op jit(solution)/shard_map/ppermute | solution.py:35
  207.8 28.8 %collective-permute-start.20 = (bf16[384,1536]{1,0:T(8,128)(2,1)S(1)}, bf16[384,1536]{1,0:T(8,128)(2,1)S(1)}, u32[]{:S(2)}, u32[]{:S(2)}) collective-permute-start(bf16[384,1536]{1,0:T(8,128)(2,1)S(1)} %copy-done.20), channel_id=1, source_target_pairs={{0,4},{4,0},{2,6},{6,2},{1,5},{5,1},{3,7},{7,3}} | collective-permute-start | bytes 3538952 | tf_op jit(solution)/shard_map/ppermute | solution.py:31
  209.3 27.7 %collective-permute-start.7 = (bf16[384,1536]{1,0:T(8,128)(2,1)}, bf16[384,1536]{1,0:T(8,128)(2,1)S(1)}, u32[]{:S(2)}, u32[]{:S(2)}) collective-permute-start(bf16[384,1536]{1,0:T(8,128)(2,1)} %collective-permute-done.6), channel_id=1, source_target_pairs={{0,1},{1,0},{2,3},{3,2},{4,5},{5,4},{6,7},{7,6}} | collective-permute-start | bytes 3538952 | tf_op jit(solution)/shard_map/ppermute | solution.py:35
  209.3 29.3 %collective-permute-start.9 = (bf16[384,1536]{1,0:T(8,128)(2,1)S(1)}, bf16[384,1536]{1,0:T(8,128)(2,1)S(1)}, u32[]{:S(2)}, u32[]{:S(2)}) collective-permute-start(bf16[384,1536]{1,0:T(8,128)(2,1)S(1)} %collective-permute-done.8), channel_id=1, source_target_pairs={{0,1},{1,0},{2,3},{3,2},{4,5},{5,4},{6,7},{7,6}} | collective-permute-start | bytes 3538952 | tf_op jit(solution)/shard_map/ppermute | solution.py:35
  212.0 30.3 %collective-permute-start.19 = (bf16[384,1536]{1,0:T(8,128)(2,1)S(1)}, bf16[384,1536]{1,0:T(8,128)(2,1)S(1)}, u32[]{:S(2)}, u32[]{:S(2)}) collective-permute-start(bf16[384,1536]{1,0:T(8,128)(2,1)S(1)} %collective-permute-done.18), channel_id=1, source_target_pairs={{0,1},{1,0},{2,3},{3,2},{4,5},{5,4},{6,7},{7,6}} | collective-permute-start | bytes 3538952 | tf_op jit(solution)/shard_map/ppermute | solution.py:35
  215.6 46.3 %collective-permute-start.10 = (bf16[384,1536]{1,0:T(8,128)(2,1)}, bf16[384,1536]{1,0:T(8,128)(2,1)S(1)}, u32[]{:S(2)}, u32[]{:S(2)}) collective-permute-start(bf16[384,1536]{1,0:T(8,128)(2,1)} %collective-permute-done.2), channel_id=1, source_target_pairs={{0,4},{4,0},{2,6},{6,2},{1,5},{5,1},{3,7},{7,3}} | collective-permute-start | bytes 3538952 | tf_op jit(solution)/shard_map/ppermute | solution.py:31
  236.6 28.8 %collective-permute-start.12 = (bf16[384,1536]{1,0:T(8,128)(2,1)S(1)}, bf16[384,1536]{1,0:T(8,128)(2,1)S(1)}, u32[]{:S(2)}, u32[]{:S(2)}) collective-permute-start(bf16[384,1536]{1,0:T(8,128)(2,1)S(1)} %collective-permute-done.8), channel_id=1, source_target_pairs={{0,2},{2,0},{4,6},{6,4},{1,3},{3,1},{5,7},{7,5}} | collective-permute-start | bytes 3538952 | tf_op jit(solution)/shard_map/ppermute | solution.py:27
  237.0 49.6 %collective-permute-start.22 = (bf16[384,1536]{1,0:T(8,128)(2,1)}, bf16[384,1536]{1,0:T(8,128)(2,1)}, u32[]{:S(2)}, u32[]{:S(2)}) collective-permute-start(bf16[384,1536]{1,0:T(8,128)(2,1)} %collective-permute-done.14), channel_id=1, source_target_pairs={{0,4},{4,0},{2,6},{6,2},{1,5},{5,1},{3,7},{7,3}} | collective-permute-start | bytes 3538952 | tf_op jit(solution)/shard_map/ppermute | solution.py:31
  238.6 50.0 %collective-permute-start.24 = (bf16[384,1536]{1,0:T(8,128)(2,1)S(1)}, bf16[384,1536]{1,0:T(8,128)(2,1)}, u32[]{:S(2)}, u32[]{:S(2)}) collective-permute-start(bf16[384,1536]{1,0:T(8,128)(2,1)S(1)} %collective-permute-done.20), channel_id=1, source_target_pairs={{0,2},{2,0},{4,6},{6,4},{1,3},{3,1},{5,7},{7,5}} | collective-permute-start | bytes 3538952 | tf_op jit(solution)/shard_map/ppermute | solution.py:27
  242.3 48.5 %collective-permute-start.21 = (bf16[384,1536]{1,0:T(8,128)(2,1)S(1)}, bf16[384,1536]{1,0:T(8,128)(2,1)S(1)}, u32[]{:S(2)}, u32[]{:S(2)}) collective-permute-start(bf16[384,1536]{1,0:T(8,128)(2,1)S(1)} %collective-permute-done.20), channel_id=1, source_target_pairs={{0,1},{1,0},{2,3},{3,2},{4,5},{5,4},{6,7},{7,6}} | collective-permute-start | bytes 3538952 | tf_op jit(solution)/shard_map/ppermute | solution.py:35
  261.9 32.4 %collective-permute-start.11 = (bf16[384,1536]{1,0:T(8,128)(2,1)S(1)}, bf16[384,1536]{1,0:T(8,128)(2,1)S(1)}, u32[]{:S(2)}, u32[]{:S(2)}) collective-permute-start(bf16[384,1536]{1,0:T(8,128)(2,1)S(1)} %collective-permute-done.10), channel_id=1, source_target_pairs={{0,1},{1,0},{2,3},{3,2},{4,5},{5,4},{6,7},{7,6}} | collective-permute-start | bytes 3538952 | tf_op jit(solution)/shard_map/ppermute | solution.py:35
  265.4 65.1 %collective-permute-start.13 = (bf16[384,1536]{1,0:T(8,128)(2,1)S(1)}, bf16[384,1536]{1,0:T(8,128)(2,1)}, u32[]{:S(2)}, u32[]{:S(2)}) collective-permute-start(bf16[384,1536]{1,0:T(8,128)(2,1)S(1)} %collective-permute-done.12), channel_id=1, source_target_pairs={{0,1},{1,0},{2,3},{3,2},{4,5},{5,4},{6,7},{7,6}} | collective-permute-start | bytes 3538952 | tf_op jit(solution)/shard_map/ppermute | solution.py:35
  286.6 39.3 %collective-permute-start.23 = (bf16[384,1536]{1,0:T(8,128)(2,1)}, bf16[384,1536]{1,0:T(8,128)(2,1)}, u32[]{:S(2)}, u32[]{:S(2)}) collective-permute-start(bf16[384,1536]{1,0:T(8,128)(2,1)} %collective-permute-done.22), channel_id=1, source_target_pairs={{0,1},{1,0},{2,3},{3,2},{4,5},{5,4},{6,7},{7,6}} | collective-permute-start | bytes 3538952 | tf_op jit(solution)/shard_map/ppermute | solution.py:35
  288.6 44.3 %collective-permute-start.25 = (bf16[384,1536]{1,0:T(8,128)(2,1)}, bf16[384,1536]{1,0:T(8,128)(2,1)}, u32[]{:S(2)}, u32[]{:S(2)}) collective-permute-start(bf16[384,1536]{1,0:T(8,128)(2,1)} %collective-permute-done.24), channel_id=1, source_target_pairs={{0,1},{1,0},{2,3},{3,2},{4,5},{5,4},{6,7},{7,6}} | collective-permute-start | bytes 3538952 | tf_op jit(solution)/shard_map/ppermute | solution.py:35
  324.2 24.4 %collective-permute-start.1 = (bf16[512,3072]{1,0:T(8,128)(2,1)}, bf16[512,3072]{1,0:T(8,128)(2,1)}, u32[]{:S(2)}, u32[]{:S(2)}) collective-permute-start(bf16[512,3072]{1,0:T(8,128)(2,1)} %get-tuple-element.108.refs_2_.refs_4_.refs_6_.refs_1_.refs_3_), channel_id=1, source_target_pairs={{0,1},{1,0},{2,3},{3,2},{4,5},{5,4},{6,7},{7,6}} | collective-permute-start | bytes 9437192 | tf_op jit(solution)/shard_map/ppermute | solution.py:35
  562.2 19.0 %collective-permute-start.28 = (bf16[512,3072]{1,0:T(8,128)(2,1)}, bf16[512,3072]{1,0:T(8,128)(2,1)}, u32[]{:S(2)}, u32[]{:S(2)}) collective-permute-start(bf16[512,3072]{1,0:T(8,128)(2,1)} %get-tuple-element.122.refs_2_.refs_4_.refs_6_.refs_1_.refs_3_), channel_id=1, source_target_pairs={{0,1},{1,0},{2,3},{3,2},{4,5},{5,4},{6,7},{7,6}} | collective-permute-start | bytes 9437192 | tf_op jit(solution)/shard_map/ppermute | solution.py:35
  717.6 10.5 collective-permute-start.30
  744.8 869.5 %all-gather.12.cloned.1.call-start = ((), (), s32[]{:S(2)}) async-start(), calls=%async_computation.11 | async-start | bytes 14155776 | tf_op jit(solution)/shard_map/all_gather | solution.py:551
  825.1 10.5 collective-permute-start.31
  852.8 777.7 %all-gather.14.cloned.1.call-start = ((), (), s32[]{:S(2)}) async-start(), calls=%async_computation.12 | async-start | bytes 14155776 | tf_op jit(solution)/shard_map/all_gather | solution.py:551
  933.0 10.5 collective-permute-start.32
  960.4 716.3 %reduce-scatter.5.cloned.1.call-start = ((), (), s32[]{:S(2)}) async-start(), calls=%async_computation.9 | async-start | bytes 21233664 | tf_op jit(solution)/shard_map/reduce_scatter | solution.py:554
  1050.7 114.5 %all-to-all-start.3 = ((bf16[8,512,768]{2,1,0:T(8,128)(2,1)}), bf16[8,512,768]{2,1,0:T(8,128)(2,1)}, u32[]{:S(2)}, u32[]{:S(2)}) async-start(bf16[8,512,768]{2,1,0:T(8,128)(2,1)} %get-tuple-element.204), calls=%async_computation.5 | async-start | bytes 12582912 | tf_op jit(solution)/shard_map/all_to_all | solution.py:598
  1054.2 664.4 %reduce-scatter.3.cloned.1.call-start = ((), (), s32[]{:S(2)}) async-start(), calls=%async_computation.8 | async-start | bytes 21233664 | tf_op jit(solution)/shard_map/reduce_scatter | solution.py:554
  1165.2 103.9 %all-to-all-start.1 = ((bf16[8,512,768]{2,1,0:T(8,128)(2,1)}), bf16[8,512,768]{2,1,0:T(8,128)(2,1)}, u32[]{:S(2)}, u32[]{:S(2)}) async-start(bf16[8,512,768]{2,1,0:T(8,128)(2,1)} %get-tuple-element.200), calls=%async_computation.3 | async-start | bytes 12582912 | tf_op jit(solution)/shard_map/all_to_all | solution.py:598
  1212.0 74.3 %collective-permute-start.33 = (f32[2,512,1536]{2,1,0:T(8,128)}, f32[2,512,1536]{2,1,0:T(8,128)}, u32[]{:S(2)}, u32[]{:S(2)}) collective-permute-start(f32[2,512,1536]{2,1,0:T(8,128)} %get-tuple-element.171), channel_id=1, source_target_pairs={{0,1},{1,0},{2,3},{3,2},{4,5},{5,4},{6,7},{7,6}} | collective-permute-start | bytes 18874376 | tf_op jit(solution)/shard_map/ppermute | solution.py:35
  1269.1 111.6 %all-to-all-start = ((bf16[8,512,768]{2,1,0:T(8,128)(2,1)}), bf16[8,512,768]{2,1,0:T(8,128)(2,1)}, u32[]{:S(2)}, u32[]{:S(2)}) async-start(bf16[8,512,768]{2,1,0:T(8,128)(2,1)} %get-tuple-element.198), calls=%async_computation.2 | async-start | bytes 12582912 | tf_op jit(solution)/shard_map/all_to_all | solution.py:598
  1306.8 23.2 %collective-permute-start.54 = (bf16[512,1536]{1,0:T(8,128)(2,1)}, bf16[512,1536]{1,0:T(8,128)(2,1)}, u32[]{:S(2)}, u32[]{:S(2)}) collective-permute-start(bf16[512,1536]{1,0:T(8,128)(2,1)} %get-tuple-element.206), channel_id=1, source_target_pairs={{0,1},{1,0},{2,3},{3,2},{4,5},{5,4},{6,7},{7,6}} | collective-permute-start | bytes 4718600 | tf_op jit(solution)/shard_map/ppermute | solution.py:35
  1329.0 23.1 %collective-permute-start.38 = (f32[2,384,768]{2,1,0:T(8,128)}, f32[2,384,768]{2,1,0:T(8,128)S(1)}, u32[]{:S(2)}, u32[]{:S(2)}) collective-permute-start(f32[2,384,768]{2,1,0:T(8,128)} %get-tuple-element.181), channel_id=1, source_target_pairs={{0,1},{1,0},{2,3},{3,2},{4,5},{5,4},{6,7},{7,6}} | collective-permute-start | bytes 7077896 | tf_op jit(solution)/shard_map/ppermute | solution.py:35
  1329.1 24.7 %collective-permute-start.39 = (f32[2,384,768]{2,1,0:T(8,128)}, f32[2,384,768]{2,1,0:T(8,128)}, u32[]{:S(2)}, u32[]{:S(2)}) collective-permute-start(f32[2,384,768]{2,1,0:T(8,128)} %get-tuple-element.182), channel_id=1, source_target_pairs={{0,1},{1,0},{2,3},{3,2},{4,5},{5,4},{6,7},{7,6}} | collective-permute-start | bytes 7077896 | tf_op jit(solution)/shard_map/ppermute | solution.py:35
  1329.5 24.5 %collective-permute-start.40 = (f32[2,384,768]{2,1,0:T(8,128)}, f32[2,384,768]{2,1,0:T(8,128)}, u32[]{:S(2)}, u32[]{:S(2)}) collective-permute-start(f32[2,384,768]{2,1,0:T(8,128)} %get-tuple-element.183), channel_id=1, source_target_pairs={{0,1},{1,0},{2,3},{3,2},{4,5},{5,4},{6,7},{7,6}} | collective-permute-start | bytes 7077896 | tf_op jit(solution)/shard_map/ppermute | solution.py:35
  1329.6 24.7 %collective-permute-start.41 = (f32[2,384,768]{2,1,0:T(8,128)}, f32[2,384,768]{2,1,0:T(8,128)}, u32[]{:S(2)}, u32[]{:S(2)}) collective-permute-start(f32[2,384,768]{2,1,0:T(8,128)} %get-tuple-element.184), channel_id=1, source_target_pairs={{0,1},{1,0},{2,3},{3,2},{4,5},{5,4},{6,7},{7,6}} | collective-permute-start | bytes 7077896 | tf_op jit(solution)/shard_map/ppermute | solution.py:35
  1330.0 128.4 %collective-permute-start.52 = (bf16[2048,1536]{1,0:T(8,128)(2,1)}, bf16[2048,1536]{1,0:T(8,128)(2,1)}, u32[]{:S(2)}, u32[]{:S(2)}) collective-permute-start(bf16[2048,1536]{1,0:T(8,128)(2,1)} %bitcast.90), channel_id=1, source_target_pairs={{0,1},{1,0},{2,3},{3,2},{4,5},{5,4},{6,7},{7,6}} | collective-permute-start | bytes 18874376 | tf_op jit(solution)/shard_map/ppermute | solution.py:35
  1353.4 61.4 %collective-permute-start.34 = (f32[2,384,768]{2,1,0:T(8,128)}, f32[2,384,768]{2,1,0:T(8,128)S(1)}, u32[]{:S(2)}, u32[]{:S(2)}) collective-permute-start(f32[2,384,768]{2,1,0:T(8,128)} %get-tuple-element.176), channel_id=1, source_target_pairs={{0,1},{1,0},{2,3},{3,2},{4,5},{5,4},{6,7},{7,6}} | collective-permute-start | bytes 7077896 | tf_op jit(solution)/shard_map/ppermute | solution.py:35
  1353.8 66.6 %collective-permute-start.35 = (f32[2,384,768]{2,1,0:T(8,128)}, f32[2,384,768]{2,1,0:T(8,128)}, u32[]{:S(2)}, u32[]{:S(2)}) collective-permute-start(f32[2,384,768]{2,1,0:T(8,128)} %get-tuple-element.177), channel_id=1, source_target_pairs={{0,1},{1,0},{2,3},{3,2},{4,5},{5,4},{6,7},{7,6}} | collective-permute-start | bytes 7077896 | tf_op jit(solution)/shard_map/ppermute | solution.py:35
  1354.0 66.4 %collective-permute-start.36 = (f32[2,384,768]{2,1,0:T(8,128)}, f32[2,384,768]{2,1,0:T(8,128)}, u32[]{:S(2)}, u32[]{:S(2)}) collective-permute-start(f32[2,384,768]{2,1,0:T(8,128)} %get-tuple-element.178), channel_id=1, source_target_pairs={{0,1},{1,0},{2,3},{3,2},{4,5},{5,4},{6,7},{7,6}} | collective-permute-start | bytes 7077896 | tf_op jit(solution)/shard_map/ppermute | solution.py:35
  1354.3 66.1 %collective-permute-start.37 = (f32[2,384,768]{2,1,0:T(8,128)}, f32[2,384,768]{2,1,0:T(8,128)}, u32[]{:S(2)}, u32[]{:S(2)}) collective-permute-start(f32[2,384,768]{2,1,0:T(8,128)} %get-tuple-element.179), channel_id=1, source_target_pairs={{0,1},{1,0},{2,3},{3,2},{4,5},{5,4},{6,7},{7,6}} | collective-permute-start | bytes 7077896 | tf_op jit(solution)/shard_map/ppermute | solution.py:35
  1380.7 107.4 %all-to-all-start.2 = ((bf16[8,512,768]{2,1,0:T(8,128)(2,1)}), bf16[8,512,768]{2,1,0:T(8,128)(2,1)}, u32[]{:S(2)}, u32[]{:S(2)}) async-start(bf16[8,512,768]{2,1,0:T(8,128)(2,1)} %get-tuple-element.202), calls=%async_computation.4 | async-start | bytes 12582912 | tf_op jit(solution)/shard_map/all_to_all | solution.py:598
  1414.8 190.2 %collective-permute-start.55 = (bf16[1024,1536]{1,0:T(8,128)(2,1)}, bf16[1024,1536]{1,0:T(8,128)(2,1)}, u32[]{:S(2)}, u32[]{:S(2)}) collective-permute-start(bf16[1024,1536]{1,0:T(8,128)(2,1)} %constant_dynamic-update-slice_fusion), channel_id=1, source_target_pairs={{0,4},{2,6},{5,1},{7,3}} | collective-permute-start | bytes 9437192 | tf_op jit(solution)/shard_map/ppermute | solution.py:647
  1420.4 174.0 %collective-permute-start.46 = (f32[2,384,768]{2,1,0:T(8,128)}, f32[2,384,768]{2,1,0:T(8,128)}, u32[]{:S(2)}, u32[]{:S(2)}) collective-permute-start(f32[2,384,768]{2,1,0:T(8,128)} %get-tuple-element.191), channel_id=1, source_target_pairs={{0,4},{4,0},{2,6},{6,2},{1,5},{5,1},{3,7},{7,3}} | collective-permute-start | bytes 7077896 | tf_op jit(solution)/shard_map/ppermute | solution.py:31
  1444.8 207.7 %collective-permute-start.45 = (f32[2,384,768]{2,1,0:T(8,128)}, f32[2,384,768]{2,1,0:T(8,128)}, u32[]{:S(2)}, u32[]{:S(2)}) collective-permute-start(f32[2,384,768]{2,1,0:T(8,128)} %get-tuple-element.189), channel_id=1, source_target_pairs={{0,4},{4,0},{2,6},{6,2},{1,5},{5,1},{3,7},{7,3}} | collective-permute-start | bytes 7077896 | tf_op jit(solution)/shard_map/ppermute | solution.py:31
  1447.0 152.2 %collective-permute-start.43 = (f32[2,384,768]{2,1,0:T(8,128)}, f32[2,384,768]{2,1,0:T(8,128)}, u32[]{:S(2)}, u32[]{:S(2)}) collective-permute-start(f32[2,384,768]{2,1,0:T(8,128)} %get-tuple-element.187), channel_id=1, source_target_pairs={{0,2},{2,0},{4,6},{6,4},{1,3},{3,1},{5,7},{7,5}} | collective-permute-start | bytes 7077896 | tf_op jit(solution)/shard_map/ppermute | solution.py:27
  1458.4 197.7 %collective-permute-start.42 = (f32[2,384,768]{2,1,0:T(8,128)}, f32[2,384,768]{2,1,0:T(8,128)}, u32[]{:S(2)}, u32[]{:S(2)}) collective-permute-start(f32[2,384,768]{2,1,0:T(8,128)} %get-tuple-element.185), channel_id=1, source_target_pairs={{0,2},{2,0},{4,6},{6,4},{1,3},{3,1},{5,7},{7,5}} | collective-permute-start | bytes 7077896 | tf_op jit(solution)/shard_map/ppermute | solution.py:27
  1597.7 54.8 %collective-permute-start.47 = (f32[2,384,768]{2,1,0:T(8,128)}, f32[2,384,768]{2,1,0:T(8,128)}, u32[]{:S(2)}, u32[]{:S(2)}) collective-permute-start(f32[2,384,768]{2,1,0:T(8,128)} %add.344), channel_id=1, source_target_pairs={{0,2},{2,0},{4,6},{6,4},{1,3},{3,1},{5,7},{7,5}} | collective-permute-start | bytes 7077896 | tf_op jit(solution)/shard_map/ppermute | solution.py:27
  1602.6 67.6 %collective-permute-start.44 = (f32[2,384,768]{2,1,0:T(8,128)}, f32[2,384,768]{2,1,0:T(8,128)}, u32[]{:S(2)}, u32[]{:S(2)}) collective-permute-start(f32[2,384,768]{2,1,0:T(8,128)} %add.341), channel_id=1, source_target_pairs={{0,4},{4,0},{2,6},{6,2},{1,5},{5,1},{3,7},{7,3}} | collective-permute-start | bytes 7077896 | tf_op jit(solution)/shard_map/ppermute | solution.py:31
  1613.7 104.9 %collective-permute-start.56 = (bf16[1024,1536]{1,0:T(8,128)(2,1)}, bf16[1024,1536]{1,0:T(8,128)(2,1)}, u32[]{:S(2)}, u32[]{:S(2)}) collective-permute-start(bf16[1024,1536]{1,0:T(8,128)(2,1)} %get-tuple-element.208), channel_id=1, source_target_pairs={{0,2},{2,0},{4,6},{6,4},{1,3},{3,1},{5,7},{7,5}} | collective-permute-start | bytes 9437192 | tf_op jit(solution)/shard_map/ppermute | solution.py:27
  1652.5 79.2 %collective-permute-start.53 = (f32[768,1536]{1,0:T(8,128)}, f32[768,1536]{1,0:T(8,128)}, u32[]{:S(2)}, u32[]{:S(2)}) collective-permute-start(f32[768,1536]{1,0:T(8,128)} %add_add_fusion.refs_0_), channel_id=1, source_target_pairs={{0,1},{1,0},{2,3},{3,2},{4,5},{5,4},{6,7},{7,6}} | collective-permute-start | bytes 14155784 | tf_op jit(solution)/shard_map/ppermute | solution.py:35
  1655.5 67.6 %collective-permute-start.49 = (f32[2,384,768]{2,1,0:T(8,128)S(1)}, f32[2,384,768]{2,1,0:T(8,128)}, u32[]{:S(2)}, u32[]{:S(2)}) collective-permute-start(f32[2,384,768]{2,1,0:T(8,128)S(1)} %add_add_fusion.1.own_b), channel_id=1, source_target_pairs={{0,1},{1,0},{2,3},{3,2},{4,5},{5,4},{6,7},{7,6}} | collective-permute-start | bytes 7077896 | tf_op jit(solution)/shard_map/ppermute | solution.py:35
  1674.4 48.8 %collective-permute-start.48 = (f32[2,384,768]{2,1,0:T(8,128)}, f32[2,384,768]{2,1,0:T(8,128)}, u32[]{:S(2)}, u32[]{:S(2)}) collective-permute-start(f32[2,384,768]{2,1,0:T(8,128)} %add_add_fusion.2.own_a), channel_id=1, source_target_pairs={{0,1},{1,0},{2,3},{3,2},{4,5},{5,4},{6,7},{7,6}} | collective-permute-start | bytes 7077896 | tf_op jit(solution)/shard_map/ppermute | solution.py:35
  1676.6 66.5 %collective-permute-start.51 = (f32[768,768]{1,0:T(8,128)}, f32[768,768]{1,0:T(8,128)}, u32[]{:S(2)}, u32[]{:S(2)}) collective-permute-start(f32[768,768]{1,0:T(8,128)} %reduce-scatter.5.cloned.1.call-done.ob_ref), channel_id=1, source_target_pairs={{0,1},{1,0},{2,3},{3,2},{4,5},{5,4},{6,7},{7,6}} | collective-permute-start | bytes 7077896 | tf_op jit(solution)/shard_map/ppermute | solution.py:35
  1718.6 24.6 %collective-permute-start.50 = (f32[768,768]{1,0:T(8,128)}, f32[768,768]{1,0:T(8,128)}, u32[]{:S(2)}, u32[]{:S(2)}) collective-permute-start(f32[768,768]{1,0:T(8,128)} %reduce-scatter.3.cloned.1.call-done.oa_ref), channel_id=1, source_target_pairs={{0,1},{1,0},{2,3},{3,2},{4,5},{5,4},{6,7},{7,6}} | collective-permute-start | bytes 7077896 | tf_op jit(solution)/shard_map/ppermute | solution.py:35
  (30 other events, 1819.4 us)
Sparse Core Ops, SparseCore 0:
  16.2 129.7 all-gather.5
  148.4 52.1 all-gather.7
  744.9 66.6 all-gather.9
  853.0 66.6 all-gather.11
  960.5 66.4 all-gather.13
  1050.8 202.9 reduce-scatter.4
  1257.3 240.5 reduce-scatter.2

commit v7 on v6

--- a/solution.py
+++ b/solution.py
@@ -85,7 +85,7 @@
         lse_ref[0, 1:2, rows] = lse[:, CHUNK:]
         ctx_t = tn(jnp.concatenate([vo_ref[...], vs_ref[...]], axis=0), pb)
         ctx_t = jnp.concatenate([ctx_t[:HEAD_DIM, :CHUNK], ctx_t[HEAD_DIM:, CHUNK:]], axis=0)
-        ctx_ref[0, rows, :] = ctx_t.T.astype(BF16)
+        ctx_ref[0, 0, rows, :] = ctx_t.T.astype(BF16)
 
     @pl.when(pl.program_id(0) == 0)
     def _():
@@ -119,9 +119,9 @@
                   pl.BlockSpec((tk, 128), nxt), pl.BlockSpec((tk, 128), nxt),
                   pl.BlockSpec((tk, 128), col(pairs)), pl.BlockSpec((tk, 128), col(pairs))]
         + [pl.BlockSpec(memory_space=pl.ANY)] * len(extra),
-        out_specs=[pl.BlockSpec((1, tq, 128), lambda j: (layer, 0, j)),
+        out_specs=[pl.BlockSpec((1, 1, tq, 128), lambda j: (3, layer, 0, j)),
                    pl.BlockSpec((1, 2, tq), lambda j: (j, 0, 0))],
-        out_shape=[jax.ShapeDtypeStruct((layers, tq, width), BF16),
+        out_shape=[jax.ShapeDtypeStruct((4, layers, tq, width), BF16),
                    jax.ShapeDtypeStruct((pairs, 2, tq), F32)],
         input_output_aliases={8: 0} if extra else {},
         scratch_shapes=[pltpu.VMEM((2 * tk, 2 * CHUNK), F32), pltpu.VMEM((2 * tk, 2 * CHUNK), F32),
@@ -134,70 +134,70 @@
     )(q, q, kv, kv_s, kv, kv_s, kv, kv_s, *extra)
 
 
-def attn_bwd_body(*refs):
-    q_ref, ko_ref, ks_ref, vo_ref, vs_ref, do_ref, lse_ref = refs[:7]
-    dq_ref, down_ref, dsib_ref = refs[-3:]
+WIDE = 256
+
+
+def attn_bwd_body(q_ref, ko_ref, ks_ref, vo_ref, vs_ref, do_ref, lse_ref, hist_ref, dq_ref, down_ref, dsib_ref):
     tk = ko_ref.shape[0]
-    k = jnp.concatenate([ko_ref[...], ks_ref[...]], axis=0)
-    v = jnp.concatenate([vo_ref[...], vs_ref[...]], axis=0)
     low = pair_masks(CHUNK)
-    for i in range(q_ref.shape[0] // CHUNK):
-        rows = slice(i * CHUNK, (i + 1) * CHUNK)
-        q = q_ref[rows, :]
-        do = do_ref[rows, :]
-        dqs = []
-        for h in range(2):
-            sel = low if h == 0 else ~low
-            qm = jnp.where(sel, q, jnp.zeros_like(q))
-            dom = jnp.where(sel, do, jnp.zeros_like(do))
-            s = nt(k, qm)
-            p = jnp.exp2(s * (SCALE * LOG2E) - lse_ref[0, h:h + 1, rows])
-            dp = nt(v, dom).astype(BF16).astype(F32)
-            delta = jnp.sum(p * dp, axis=0, keepdims=True)
-            ds = (p * (dp - delta)).astype(BF16)
-            dv = nn(p.astype(BF16), dom)
-            dk = nn(ds, qm) * SCALE
-            for n, grad in enumerate((dk, dv)):
-                for ref, part in ((down_ref, grad[:tk]), (dsib_ref, grad[tk:])):
-                    if i == 0 and h == 0:
-                        ref[n] = part
-                    else:
-                        ref[n] += part
-            dqs.append(tn(k, ds)[h * HEAD_DIM:(h + 1) * HEAD_DIM, :] * SCALE)
-        dq_ref[0, rows, :] = jnp.concatenate(dqs, axis=0).T.astype(BF16)
+    for sub in range(WIDE // 128):
+        cols = slice(sub * 128, (sub + 1) * 128)
+        k = jnp.concatenate([ko_ref[:, cols], ks_ref[:, cols]], axis=0)
+        v = jnp.concatenate([vo_ref[:, cols], vs_ref[:, cols]], axis=0)
+        for i in range(q_ref.shape[0] // CHUNK):
+            rows = slice(i * CHUNK, (i + 1) * CHUNK)
+            q = q_ref[rows, cols]
+            do = do_ref[rows, cols]
+            dqs = []
+            for h in range(2):
+                sel = low if h == 0 else ~low
+                qm = jnp.where(sel, q, jnp.zeros_like(q))
+                dom = jnp.where(sel, do, jnp.zeros_like(do))
+                s = nt(k, qm)
+                p = jnp.exp2(s * (SCALE * LOG2E) - lse_ref[sub, h:h + 1, rows])
+                dp = nt(v, dom).astype(BF16).astype(F32)
+                delta = jnp.sum(p * dp, axis=0, keepdims=True)
+                ds = (p * (dp - delta)).astype(BF16)
+                dv = nn(p.astype(BF16), dom)
+                dk = nn(ds, qm) * SCALE
+                for n, grad in enumerate((dk, dv)):
+                    for ref, part in ((down_ref, grad[:tk]), (dsib_ref, grad[tk:])):
+                        if i == 0 and h == 0:
+                            ref[n, :, cols] = part
+                        else:
+                            ref[n, :, cols] += part
+                dqs.append(tn(k, ds)[h * HEAD_DIM:(h + 1) * HEAD_DIM, :] * SCALE)
+            dq_ref[0, 0, rows, cols] = jnp.concatenate(dqs, axis=0).T.astype(BF16)
 
 
 def attn_bwd(q, kv, kv_s, d_ctx, lse, layer, layers, hist):
     tq, width = q.shape
     tk = kv.shape[0]
-    pairs = width // 128
+    steps = width // WIDE
 
     def col(off):
         return lambda j: (0, j + off)
 
     flops = 5 * 2 * tq * (2 * tk) * 256 * (width // HEAD_DIM)
-    kblk = pl.BlockSpec((tk, 128), col(0))
-    both = pl.BlockSpec((2, tk, 128), lambda j: (0, 0, j))
-    extra = [] if hist is None else [hist]
+    qblk = pl.BlockSpec((tq, WIDE), col(0))
+    kblk = pl.BlockSpec((tk, WIDE), col(0))
+    vblk = pl.BlockSpec((tk, WIDE), col(steps))
+    both = pl.BlockSpec((2, tk, WIDE), lambda j: (0, 0, j))
     return pl.pallas_call(
         attn_bwd_body,
-        grid=(pairs,),
-        in_specs=[pl.BlockSpec((tq, 128), col(0)),
-                  kblk, kblk,
-                  pl.BlockSpec((tk, 128), col(pairs)), pl.BlockSpec((tk, 128), col(pairs)),
-                  pl.BlockSpec((tq, 128), col(0)),
-                  pl.BlockSpec((1, 2, tq), lambda j: (j, 0, 0))]
-        + [pl.BlockSpec(memory_space=pl.ANY)] * len(extra),
-        out_specs=[pl.BlockSpec((1, tq, 128), lambda j: (layer, 0, j)), both, both],
-        out_shape=[jax.ShapeDtypeStruct((layers, tq, width), BF16)]
+        grid=(steps,),
+        in_specs=[qblk, kblk, kblk, vblk, vblk, qblk,
+                  pl.BlockSpec((WIDE // 128, 2, tq), lambda j: (j, 0, 0)), pl.BlockSpec(memory_space=pl.ANY)],
+        out_specs=[pl.BlockSpec((1, 1, tq, WIDE), lambda j: (0, layer, 0, j)), both, both],
+        out_shape=[jax.ShapeDtypeStruct((4, layers, tq, width), BF16)]
         + [jax.ShapeDtypeStruct((2, tk, width), F32)] * 2,
-        input_output_aliases={7: 0} if extra else {},
+        input_output_aliases={7: 0},
         compiler_params=pltpu.CompilerParams(dimension_semantics=('arbitrary',),
                                              vmem_limit_bytes=VMEM_ALL),
         cost_estimate=pl.CostEstimate(flops=flops, bytes_accessed=2 * (2 * tq * width * 2 + 4 * tk * width) + 16 * tk * width,
                                       transcendentals=tq * 2 * tk * (width // HEAD_DIM)),
         name='attn_bwd',
-    )(q, kv, kv_s, kv, kv_s, d_ctx, lse, *extra)
+    )(q, kv, kv_s, kv, kv_s, d_ctx, lse, hist)
 
 
 def kv_body(*refs):
@@ -207,10 +207,10 @@
     @pl.when(pl.program_id(0) == 0)
     def _():
         s = x_ref[...].astype(F32) + e_ref[...]
-        u_ref[0] = (s * lax.rsqrt(jnp.mean(s * s, axis=-1, keepdims=True) + EPS_NORM)).astype(BF16)
+        u_ref[0, 0] = (s * lax.rsqrt(jnp.mean(s * s, axis=-1, keepdims=True) + EPS_NORM)).astype(BF16)
 
     for rows in ROWS:
-        kv_ref[rows, :] = nt(u_ref[0, rows, :], w_ref[...]).astype(BF16)
+        kv_ref[rows, :] = nt(u_ref[0, 0, rows, :], w_ref[...]).astype(BF16)
 
 
 def norm_kv(x, e, wkv, layer, layers, hist):
@@ -223,8 +223,8 @@
         grid=(width // blk,),
         in_specs=[pl.BlockSpec((t, dim), lambda j: (0, 0)), pl.BlockSpec((1, dim), lambda j: (0, 0)),
                   pl.BlockSpec((blk, dim), lambda j: (j, 0))] + [pl.BlockSpec(memory_space=pl.ANY)] * len(extra),
-        out_specs=[pl.BlockSpec((t, blk), lambda j: (0, j)), pl.BlockSpec((1, t, dim), lambda j: (layer, 0, 0))],
-        out_shape=[jax.ShapeDtypeStruct((t, width), BF16), jax.ShapeDtypeStruct((layers, t, dim), BF16)],
+        out_specs=[pl.BlockSpec((t, blk), lambda j: (0, j)), pl.BlockSpec((1, 1, t, dim), lambda j: (0, layer, 0, 0))],
+        out_shape=[jax.ShapeDtypeStruct((t, width), BF16), jax.ShapeDtypeStruct((2, layers, t, dim), BF16)],
         input_output_aliases={3: 1} if extra else {},
         compiler_params=pltpu.CompilerParams(dimension_semantics=('arbitrary',), vmem_limit_bytes=VMEM_ALL),
         cost_estimate=pl.CostEstimate(flops=2 * t * dim * width, bytes_accessed=2 * (dim * width + t * width + 2 * t * dim),
@@ -233,25 +233,16 @@
     )(x, e, wkv, *extra)
 
 
-def d_kv_body(*refs):
-    acc0_ref, x_ref, e_ref, mid_ref, own_ref, recv_ref, w_ref = refs[:7]
-    dk_ref, dv_ref, prev_ref, acc_ref = refs[-4:]
+def d_kv_body(acc0_ref, x_ref, e_ref, mid_ref, own_ref, recv_ref, w_ref, hist_ref, dkv_ref, prev_ref, acc_ref):
     j = pl.program_id(0)
 
     @pl.when(j == 0)
     def _():
         acc_ref[...] = acc0_ref[...]
 
-    grad = (own_ref[0] + recv_ref[0]).astype(BF16)
-    half = grad.shape[1]
-    for n, ref in enumerate((dk_ref, dv_ref)):
-        for part in range(2):
-            @pl.when(j == 2 * n + part)
-            def _():
-                ref[0, :, part * half:(part + 1) * half] = grad
-
+    dkv_ref[0, 0] = (own_ref[0] + recv_ref[0]).astype(BF16)
     for rows in ROWS:
-        acc_ref[rows, :] += nn(grad[rows, :], w_ref[...])
+        acc_ref[rows, :] += nn(dkv_ref[0, 0, rows, :], w_ref[...])
 
     @pl.when(j == pl.num_programs(0) - 1)
     def _():
@@ -259,64 +250,88 @@
         s = x_ref[...].astype(F32) + e_ref[...]
         inv = lax.rsqrt(jnp.mean(s * s, axis=-1, keepdims=True) + EPS_NORM)
         proj = jnp.mean(s * dn, axis=-1, keepdims=True)
-        prev_ref[...] = (mid_ref[0].astype(F32) + inv * dn - s * (inv * inv * inv * proj)).astype(BF16)
-
-
-def d_kv(acc0, x, e, mid_hist, own, recv, wkv, layer, layers, dk_hist, dv_hist):
+        prev_ref[...] = (mid_ref[0, 0].astype(F32) + inv * dn - s * (inv * inv * inv * proj)).astype(BF16)
+
+
+def d_kv(acc0, x, e, um_hist, own, recv, wkv, layer, layers, hist):
     t, dim = x.shape
     half = dim // 2
     whole = pl.BlockSpec((t, dim), lambda j: (0, 0))
-    slab = pl.BlockSpec((1, t, dim), lambda j: (layer, 0, 0))
     gblk = pl.BlockSpec((1, t, half), lambda j: (j // 2, 0, j % 2))
-    extra = [] if dk_hist is None else [dk_hist, dv_hist]
     return pl.pallas_call(
         d_kv_body,
         grid=(4,),
-        in_specs=[whole, whole, pl.BlockSpec((1, dim), lambda j: (0, 0)), slab, gblk, gblk,
-                  pl.BlockSpec((half, dim), lambda j: (j, 0))] + [pl.BlockSpec(memory_space=pl.ANY)] * len(extra),
-        out_specs=[slab, slab, whole],
-        out_shape=[jax.ShapeDtypeStruct((layers, t, dim), BF16)] * 2 + [jax.ShapeDtypeStruct((t, dim), BF16)],
+        in_specs=[whole, whole, pl.BlockSpec((1, dim), lambda j: (0, 0)),
+                  pl.BlockSpec((1, 1, t, dim), lambda j: (1, layer, 0, 0)), gblk, gblk,
+                  pl.BlockSpec((half, dim), lambda j: (j, 0)), pl.BlockSpec(memory_space=pl.ANY)],
+        out_specs=[pl.BlockSpec((1, 1, t, half), lambda j: (1 + j // 2, layer, 0, j % 2)), whole],
+        out_shape=[jax.ShapeDtypeStruct((4, layers, t, dim), BF16), jax.ShapeDtypeStruct((t, dim), BF16)],
         scratch_shapes=[pltpu.VMEM((t, dim), F32)],
-        input_output_aliases={7: 0, 8: 1} if extra else {},
+        input_output_aliases={7: 0},
         compiler_params=pltpu.CompilerParams(dimension_semantics=('arbitrary',), vmem_limit_bytes=VMEM_ALL),
         cost_estimate=pl.CostEstimate(flops=4 * t * dim * dim, bytes_accessed=4 * dim * dim + 20 * t * dim, transcendentals=t),
         name='d_kv',
-    )(acc0, x, e, mid_hist, own, recv, wkv, *extra)
-
-
-def terms_body(added, *refs):
-    lhs, rhs, recv, outs = refs[:4], (refs[4], refs[4], refs[4], refs[5]), refs[6:6 + 4 * added], refs[-4:]
-    r, kind = pl.program_id(0), pl.program_id(1)
-    for n in range(4):
-        @pl.when(kind == n)
+    )(acc0, x, e, um_hist, own, recv, wkv, hist)
+
+
+def terms_body(added, places_ref, lhs_ref, rhs_ref, *refs):
+    recv, outs = refs[:4 * added], refs[-4:]
+    step = 4 * pl.program_id(0) + pl.program_id(1)
+    val = tn(lhs_ref[0], rhs_ref[0])
+    for slot in range(4):
+        @pl.when(step // 2 == slot)
         def _():
-            val = tn(lhs[n][...], rhs[n][...])
-            for c in range(2):
-                @pl.when(r == c)
-                def _():
-                    slot = 2 * c + n // 2
-                    outs[slot][0] = val + recv[slot][0] if added else val
-
-
-def terms(dq, dk, dv, ctx, u_half, mid_half, chips, recv):
-    tokens, dim = dq.shape
-    hid = dim // 4
-    half_d = u_half.shape[1]
+            outs[slot][0] = val + recv[slot][0] if added else val
+
+
+def terms(lhs, rhs, rows, cols, places, lhs_at, rhs_at, chips, recv):
+    tokens = lhs.shape[1]
     first, second = chips
-    whole = pl.BlockSpec((tokens, half_d), lambda r, kind: (0, 0))
-    src = pl.BlockSpec((tokens, hid), lambda r, kind: (0, first + r * (second - first)))
-    slots = [pl.BlockSpec((1, hid, half_d), lambda r, kind, at=2 * n: (jnp.clip(4 * r + kind - at, 0, 1), 0, 0))
+
+    def rel(r):
+        return first + r * (second - first)
+
+    slots = [pl.BlockSpec((1, rows, cols), lambda r, kind, p, at=2 * n: (jnp.clip(4 * r + kind - at, 0, 1), 0, 0))
              for n in range(4)]
     out = pl.pallas_call(
         functools.partial(terms_body, len(recv) // 4),
-        grid=(2, 4),
-        in_specs=[src] * 4 + [whole] * 2 + slots[:len(recv)],
-        out_specs=slots,
-        out_shape=[jax.ShapeDtypeStruct((2, hid, half_d), F32)] * 4,
+        grid_spec=pltpu.PrefetchScalarGridSpec(
+            num_scalar_prefetch=1, grid=(2, 4),
+            in_specs=[pl.BlockSpec((1, tokens, rows), lambda r, kind, p: lhs_at(rel(r), kind, p)),
+                      pl.BlockSpec((1, tokens, cols), lambda r, kind, p: rhs_at(rel(r), kind, p))] + slots[:len(recv)],
+            out_specs=slots),
+        out_shape=[jax.ShapeDtypeStruct((2, rows, cols), F32)] * 4,
         compiler_params=pltpu.CompilerParams(dimension_semantics=('arbitrary', 'arbitrary'), vmem_limit_bytes=VMEM_ALL),
-        cost_estimate=pl.CostEstimate(flops=16 * tokens * hid * half_d, bytes_accessed=24 * tokens * hid, transcendentals=0),
-    )(dq, dk, dv, ctx, u_half, mid_half, *recv)
+        cost_estimate=pl.CostEstimate(flops=16 * tokens * rows * cols, bytes_accessed=24 * tokens * rows, transcendentals=0),
+    )(places, lhs, rhs, *recv)
     return {first: out[:2], second: out[2:]}
+
+
+def attn_lhs_at(rel, kind, p):
+    return kind, 0, rel
+
+
+def attn_rhs_at(rel, kind, p):
+    return kind // 3, 0, p[0]
+
+
+def up_lhs_at(rel, kind, p):
+    return 0, 0, 4 * p[1 + rel] + 2 * p[0] + kind % 2
+
+
+def up_rhs_at(rel, kind, p):
+    return 0, 0, kind // 2
+
+
+def summed_terms(lhs, rhs, rows, cols, places, lhs_at, rhs_at):
+    sent = {}
+    for pair in ((3, 1), (2, 0)):
+        for r, ab in terms(lhs, rhs, rows, cols, places[1], lhs_at, rhs_at, pair, []).items():
+            sent[r] = [pp_d(v) for v in ab]
+    total = {}
+    for pair in ((3, 1), (2, 0)):
+        total.update(terms(lhs, rhs, rows, cols, places[0], lhs_at, rhs_at, pair, sent[pair[0]] + sent[pair[1]]))
+    return total
 
 
 GELU_C = 0.7978845608028654
@@ -334,7 +349,7 @@
     def _():
         for rows in ROWS:
             s = x0_ref[rows, :].astype(F32) + e_ref[...]
-            h = (s + nn(ctx_ref[0, rows, :], wo_ref[...])).astype(BF16)
+            h = (s + nn(ctx_ref[0, 0, rows, :], wo_ref[...])).astype(BF16)
             h_ref[rows, :] = h
             hf = h.astype(F32)
             acc_ref[rows, :] = hf
@@ -365,7 +380,8 @@
     return pl.pallas_call(
         mlp_fwd_body,
         grid=(hidden // BLOCK_F,),
-        in_specs=[whole, pl.BlockSpec((1, dim), lambda j: (0, 0)), slab, pl.BlockSpec((dim, dim), lambda j: (0, 0)), wblk, wblk]
+        in_specs=[whole, pl.BlockSpec((1, dim), lambda j: (0, 0)), pl.BlockSpec((1, 1, t, dim), lambda j: (3, layer, 0, 0)),
+                  pl.BlockSpec((dim, dim), lambda j: (0, 0)), wblk, wblk]
         + [pl.BlockSpec(memory_space=pl.ANY)] * len(extra),
         out_specs=[pl.BlockSpec((t, BLOCK_F), lambda j: (0, j)),
                    pl.BlockSpec((1, t, BLOCK_F), lambda j: (j, 0, 0)), whole, whole, slab],
@@ -415,26 +431,26 @@
             inv = lax.rsqrt(jnp.mean(hf * hf, axis=-1, keepdims=True) + EPS_NORM)
             proj = jnp.mean(hf * dn, axis=-1, keepdims=True)
             mid = (d_ref[rows, :].astype(F32) + inv * dn - hf * (inv * inv * inv * proj)).astype(BF16)
-            mid_ref[0, rows, :] = mid
+            mid_ref[0, 0, rows, :] = mid
             dctx_ref[rows, :] = nt(mid, wo_ref[...]).astype(BF16)
 
 
-def mlp_bwd(d_next, h, z, wo, w1t, w2, layer, layers, hist, mid_hist):
+def mlp_bwd(d_next, h, z, wo, w1t, w2, layer, layers, um_hist, hist):
     t, dim = h.shape
     hidden = w2.shape[0]
     whole = pl.BlockSpec((t, dim), lambda j: (0, 0))
     wblk = pl.BlockSpec((BLOCK_B, dim), lambda j: (j, 0))
-    extra = [] if hist is None else [hist, mid_hist]
+    extra = [um_hist] if hist is None else [um_hist, hist]
     return pl.pallas_call(
         mlp_bwd_body,
         grid=(hidden // BLOCK_B,),
         in_specs=[whole, whole, pl.BlockSpec((t, BLOCK_B), lambda j: (0, j)), pl.BlockSpec((dim, dim), lambda j: (0, 0)), wblk, wblk]
         + [pl.BlockSpec(memory_space=pl.ANY)] * len(extra),
-        out_specs=[pl.BlockSpec((1, t, BLOCK_B), lambda j: (layer, 0, j)), pl.BlockSpec((1, t, dim), lambda j: (layer, 0, 0)), whole],
-        out_shape=[jax.ShapeDtypeStruct((layers, t, hidden), BF16), jax.ShapeDtypeStruct((layers, t, dim), BF16),
+        out_specs=[pl.BlockSpec((1, t, BLOCK_B), lambda j: (layer, 0, j)), pl.BlockSpec((1, 1, t, dim), lambda j: (1, layer, 0, 0)), whole],
+        out_shape=[jax.ShapeDtypeStruct((layers, t, hidden), BF16), jax.ShapeDtypeStruct((2, layers, t, dim), BF16),
                    jax.ShapeDtypeStruct((t, dim), BF16)],
         scratch_shapes=[pltpu.VMEM((t, dim), F32)],
-        input_output_aliases={6: 0, 7: 1} if extra else {},
+        input_output_aliases={6: 1} if hist is None else {6: 1, 7: 0},
         compiler_params=pltpu.CompilerParams(dimension_semantics=('arbitrary',), vmem_limit_bytes=VMEM_ALL),
         cost_estimate=pl.CostEstimate(flops=4 * t * dim * hidden, bytes_accessed=4 * dim * hidden + 4 * t * hidden,
                                       transcendentals=t * hidden),
@@ -550,9 +566,6 @@
         def gather(v):
             return lax.all_gather(v, BOTH, axis=0, tiled=True)
 
-        def scatter(v):
-            return lax.psum_scatter(v, BOTH, scatter_dimension=0, tiled=True)
-
         def after(v, *deps):
             return lax.optimization_barrier((v,) + deps)[0]
 
@@ -587,22 +600,23 @@
 
         saved = []
         g_mine = []
-        u_hist = m_hist = ctx_hist = None
+        um_hist = m_hist = att_hist = None
         for layer in range(layer_count):
             e = emb[layer:layer + 1]
-            kv, u_hist = norm_kv(x_cur, e, wkv, layer, layer_count, u_hist)
+            kv, um_hist = norm_kv(x_cur, e, wkv, layer, layer_count, um_hist)
             kv_s = pp_d(kv)
-            q = nt(u_hist[layer], wq).astype(BF16)
-            ctx_hist, lse = attn_fwd(q, kv, kv_s, layer, layer_count, ctx_hist)
-            z, g, x_next, h, m_hist = mlp_fwd(x_cur, e, ctx_hist, wo, w1, w2, layer, layer_count, m_hist)
+            q = nt(um_hist[0, layer], wq).astype(BF16)
+            att_hist, lse = attn_fwd(q, kv, kv_s, layer, layer_count, att_hist)
+            z, g, x_next, h, m_hist = mlp_fwd(x_cur, e, att_hist, wo, w1, w2, layer, layer_count, m_hist)
             g_mine.append(lax.all_to_all(g.reshape(-1, g.shape[-1]), BOTH, split_axis=0, concat_axis=0, tiled=True))
             saved.append((x_cur, q, kv, kv_s, lse, h, z))
             x_cur = x_next
 
-        def flat(v):
-            return v.reshape(-1, v.shape[-1])
-
-        up_hist = mid_hist = dq_hist = dk_hist = dv_hist = None
+        def flat(v, lead):
+            return v.reshape(lead, -1, v.shape[-1])
+
+        places = [jnp.stack([w, *chips]).astype(jnp.int32) for w in (core, 1 - core)]
+        up_hist = None
         next_all = [None] * layer_count
         for layer in reversed(range(layer_count)):
             x_l, q, kv, kv_s, lse, h, z = saved[layer]
@@ -610,29 +624,18 @@
             d_next = d_cur
             if layer < layer_count - 1:
                 next_all[layer] = gather(d_next)
-            up_hist, mid_hist, d_ctx = mlp_bwd(d_next, h, z, wo, w1, w2, layer, layer_count, up_hist, mid_hist)
+            up_hist, um_hist, d_ctx = mlp_bwd(d_next, h, z, wo, w1, w2, layer, layer_count, um_hist, up_hist)
             if layer == 0:
-                up_f, m_f = flat(up_hist), flat(m_hist)
-                term_1a, d_ctx, up_f = lax.optimization_barrier((tn(up_f, m_f[:, :half_d]), d_ctx, up_f))
-                grad_1a = scatter(term_1a)
-                term_1b = tn(up_f, m_f[:, half_d:])
-                term_1b, d_ctx = lax.optimization_barrier((term_1b, d_ctx))
-                grad_1b = scatter(term_1b)
-            dq_hist, own_kv, sib_kv = attn_bwd(q, kv, kv_s, d_ctx, lse, layer, layer_count, dq_hist)
+                total = summed_terms(flat(up_hist, 1), flat(m_hist, 1), hid, half_d, places, up_lhs_at, up_rhs_at)
+                d_ctx = after(d_ctx, *[v for r in (1, 2, 3) for v in total[r]])
+                own_1a = reduce_terms({r: v[0] for r, v in total.items()}, pp_x, pp_y, 1, 2)
+                own_1b = reduce_terms({r: v[1] for r, v in total.items()}, pp_y, pp_x, 2, 1)
+            att_hist, own_kv, sib_kv = attn_bwd(q, kv, kv_s, d_ctx, lse, layer, layer_count, att_hist)
             recv_kv = pp_d(sib_kv)
-            acc0 = nn(dq_hist[layer], wq)
-            dk_hist, dv_hist, d_cur = d_kv(acc0, x_l, e, mid_hist, own_kv, recv_kv, wkv, layer, layer_count, dk_hist, dv_hist)
-
-        mid_half = [lax.optimization_barrier(take(flat(mid_hist), w, 1, half_d)) for w in (core, 1 - core)]
-        u_half = [lax.optimization_barrier(take(flat(u_hist), w, 1, half_d)) for w in (core, 1 - core)]
-        lhs = [flat(v) for v in (dq_hist, dk_hist, dv_hist, ctx_hist)]
-        sent = {}
-        for pair in ((3, 1), (2, 0)):
-            for r, ab in terms(*lhs, u_half[1], mid_half[1], pair, []).items():
-                sent[r] = [pp_d(v) for v in ab]
-        total = {}
-        for pair in ((3, 1), (2, 0)):
-            total.update(terms(*lhs, u_half[0], mid_half[0], pair, sent[pair[0]] + sent[pair[1]]))
+            acc0 = nn(att_hist[0, layer], wq)
+            att_hist, d_cur = d_kv(acc0, x_l, e, um_hist, own_kv, recv_kv, wkv, layer, layer_count, att_hist)
+
+        total = summed_terms(flat(att_hist, 4), flat(um_hist, 2), hid, half_d, places, attn_lhs_at, attn_rhs_at)
         own_qk = reduce_terms({r: v[0] for r, v in total.items()}, pp_x, pp_y, 1, 2)
         own_vo = reduce_terms({r: v[1] for r, v in total.items()}, pp_y, pp_x, 2, 1)
 
@@ -663,7 +666,8 @@
                 grad_2 = grad_2 + tn(g_all, next_all[layer])
 
         grad_2 = join(core, grad_2, pp_d(grad_2))
-        grad_1 = join_flip(core, [grad_1a, grad_1b], [pp_d(grad_1a), pp_d(grad_1b)])
+        own_1 = [v.reshape(-1, half_d) for v in (own_1a, own_1b)]
+        grad_1 = join_flip(core, own_1, [pp_d(v) for v in own_1])
         gq, gk, gv, go = join_attn(core, (own_qk, own_vo), (pp_d(own_qk), pp_d(own_vo)))
         return gq, gk, gv, go, grad_1, grad_2, d_x
 

time: 1760 us -> 1810 us (1.028)
  Pallas kernels: 781 us -> 852 us
  matrix products: 179 us -> 125 us
  waiting for transfers between devices: 566 us -> 588 us
    all_to_all x4, waiting for transfers between devices: 206 us -> 123 us  [device_step(): lax.all_to_all(g.reshape(-1, g.shape[-1]), BOTH, split_axis=0, concat_axi...]
    pallas_call x8 -> x12, Pallas kernels: 264 us -> 343 us  [the longest x8 175 us: terms(): pl.pallas_call(functools.partial(terms_body, len(recv) // 4), grid_spec=p...]
    dot_general x15 -> x13, matrix products: 179 us -> 125 us  [dot(): return lax.dot_general(a, b, (dims, ((), ())), preferred_element_type=F32)]
    ppermute x9 -> x12, waiting for transfers between devices: 161 us -> 215 us  [pp_y(): return lax.ppermute(v, 'model', SWAP_Y)]
    ppermute x1, waiting for transfers between devices: 0.01 us -> 34.8 us  [device_step(): from_y = lax.ppermute(whole, BOTH, to_row)]
    ppermute x10 -> x13, waiting for transfers between devices: 178 us -> 195 us  [pp_x(): return lax.ppermute(v, 'model', SWAP_X)]
  transfers between devices with their start and end apart: 68 -> 80, of which waited for: 22 -> 24; matrix products, arithmetic and copies ran while one was open for 19% -> 15% of each run, Pallas kernels for 24% -> 27%
where the time goes in v7:
time: 1810 us; the launch traced here: 1800 us
  Pallas kernels  852 us (47%)
  waiting for transfers between devices  588 us (32%)
  matrix products  125 us (7%)
  local copies, waits for them, and re-layouts  116 us (6%)
  starting transfers between devices  59.8 us (3%)
  other arithmetic  48.5 us (3%)
    ppermute x12, waiting for transfers between devices, pp_y(): return lax.ppermute(v, 'model', SWAP_Y)  215 us
    ppermute x13, waiting for transfers between devices, pp_x(): return lax.ppermute(v, 'model', SWAP_X)  195 us
    pallas_call x8, Pallas kernels, terms(): pl.pallas_call(functools.partial(terms_body, len(recv) // 4), grid_spec=p...  175 us
    pallas_call x4, Pallas kernels, attn_bwd(): pl.pallas_call(attn_bwd_body, grid=(steps,), in_specs=[qblk, kblk, kblk,...  168 us
    pallas_call x4, Pallas kernels, mlp_bwd(): pl.pallas_call(mlp_bwd_body, grid=(hidden // BLOCK_B,), in_specs=[whole,...  147 us
    pallas_call x4, Pallas kernels, mlp_fwd(): pl.pallas_call(mlp_fwd_body, grid=(hidden // BLOCK_F,), in_specs=[whole,...  134 us
    dot_general x13, matrix products, dot(): return lax.dot_general(a, b, (dims, ((), ())), preferred_element_type=F32)  125 us
    all_to_all x4, waiting for transfers between devices, device_step(): lax.all_to_all(g.reshape(-1, g.shape[-1]), BOTH, split_axis=0, concat_axi...  123 us
  transfers between devices with their start and end apart: 80, of which 24 were waited for; matrix products, arithmetic and copies ran while one was open for 15% of the time, Pallas kernels for 27%

profile of v7, /device:TPU:0, one launch (start us, length us, event | category | flops | bytes accessed | tf_op | source)
XLA Modules:
  0.0 1804.0 jit_solution(17119667737347255688)
XLA Ops:
  16.2 6.6 copy.43
  39.6 7.3 broadcast.6.clone
  50.0 26.6 %collective-permute-done.2 = bf16[384,1536]{1,0:T(8,128)(2,1)} collective-permute-done((bf16[384,1536]{1,0:T(8,128)(2,1)}, bf16[384,1536]{1,0:T(8,128)(2,1)}, u32[]{:S(2)}, u32[]{:S(2)}) %collective-permute-start.2) | collective-permute-done | bytes 1179680 | tf_op jit(solution)/shard_map/ppermute | solution.py:27
  77.1 6.6 broadcast.6.clone.1
  86.1 41.1 %collective-permute-done.4 = bf16[384,1536]{1,0:T(8,128)(2,1)} collective-permute-done((bf16[384,1536]{1,0:T(8,128)(2,1)}, bf16[384,1536]{1,0:T(8,128)(2,1)}, u32[]{:S(2)}, u32[]{:S(2)}) %collective-permute-start.4) | collective-permute-done | bytes 1179680 | tf_op jit(solution)/shard_map/ppermute | solution.py:27
  131.7 34.3 %collective-permute-done.14 = bf16[384,1536]{1,0:T(8,128)(2,1)} collective-permute-done((bf16[384,1536]{1,0:T(8,128)(2,1)}, bf16[384,1536]{1,0:T(8,128)(2,1)}, u32[]{:S(2)}, u32[]{:S(2)}) %collective-permute-start.14) | collective-permute-done | bytes 1179680 | tf_op jit(solution)/shard_map/ppermute | solution.py:27
  175.3 29.9 %collective-permute-done.16 = bf16[384,1536]{1,0:T(8,128)(2,1)S(1)} collective-permute-done((bf16[384,1536]{1,0:T(8,128)(2,1)S(1)}, bf16[384,1536]{1,0:T(8,128)(2,1)S(1)}, u32[]{:S(2)}, u32[]{:S(2)}) %collective-permute-start.16) | collective-permute-done | bytes 1179680 | tf_op jit(solution)/shard_map/ppermute | solution.py:27
  217.2 19.4 %collective-permute-done.20 = bf16[384,1536]{1,0:T(8,128)(2,1)S(1)} collective-permute-done((bf16[384,1536]{1,0:T(8,128)(2,1)S(1)}, bf16[384,1536]{1,0:T(8,128)(2,1)S(1)}, u32[]{:S(2)}, u32[]{:S(2)}) %collective-permute-start.20) | collective-permute-done | bytes 1179680 | tf_op jit(solution)/shard_map/ppermute | solution.py:31
  244.6 17.3 collective-permute-done.10
  265.4 21.1 %collective-permute-done.22 = bf16[384,1536]{1,0:T(8,128)(2,1)} collective-permute-done((bf16[384,1536]{1,0:T(8,128)(2,1)}, bf16[384,1536]{1,0:T(8,128)(2,1)}, u32[]{:S(2)}, u32[]{:S(2)}) %collective-permute-start.22) | collective-permute-done | bytes 1179680 | tf_op jit(solution)/shard_map/ppermute | solution.py:31
  313.4 10.8 norm_kv.4
  340.8 7.8 convolution_convert_fusion.3.refs_0_.refs_1_.q_ref
  348.6 23.9 %attn_fwd.4 = (bf16[4,4,512,1536]{3,2,1,0:T(8,128)(2,1)}, f32[12,2,512]{2,1,0:T(2,128)}) custom-call(bf16[512,1536]{1,0:T(8,128)(2,1)} %convolution_convert_fusion.3.refs_0_.refs_1_.q_ref, bf16[512,1536]{1,0:T(8,128)(2,1)} %convolution_convert_fusion.3.refs_0_.refs_1_.q_ref, bf16[512,3072]{1,0:T(8,128)(2,1)} %get-tuple-element.116.refs_2_.refs_4_.refs_6_.ko_ref.vo_ref, ...), custom_call_target="tpu_custom_call" | custom-call | flops 12884901888 | bytes 9437184 | tf_op jit(solution)/shard_map/attn_fwd/pallas_call | solution.py:114
  372.5 33.6 %mlp_fwd.4 = (bf16[512,6144]{1,0:T(8,128)(2,1)}, bf16[8,512,768]{2,1,0:T(8,128)(2,1)}, bf16[512,1536]{1,0:T(8,128)(2,1)}, bf16[512,1536]{1,0:T(8,128)(2,1)}, bf16[4,512,1536]{2,1,0:T(8,128)(2,1)}) custom-call(bf16[512,1536]{1,0:T(8,128)(2,1)} %bitcast_select_fusion.1.refs_0_.x_ref, f32[1,1536]{1,0:T(1,128)} %get-tuple-element.241.refs_1_.e_ref, ...), custom_call_target="tpu_custom_call" | custom-call | flops 19327352832 | bytes 50331648 | tf_op jit(solution)/shard_map/mlp_fwd/pallas_call | solution.py:380
  406.1 10.0 norm_kv.5
  422.1 23.5 %attn_fwd.5 = (bf16[4,4,512,1536]{3,2,1,0:T(8,128)(2,1)}, f32[12,2,512]{2,1,0:T(2,128)}) custom-call(bf16[512,1536]{1,0:T(8,128)(2,1)} %convolution_convert_fusion.2.refs_0_.refs_1_.q_ref, bf16[512,1536]{1,0:T(8,128)(2,1)} %convolution_convert_fusion.2.refs_0_.refs_1_.q_ref, ...), custom_call_target="tpu_custom_call", output_to_operand_aliasing={{0}: (8, {})} | custom-call | flops 12884901888 | bytes 9437184 | tf_op jit(solution)/shard_map/attn_fwd/pallas_call | solution.py:114
  445.6 33.6 %mlp_fwd.5 = (bf16[512,6144]{1,0:T(8,128)(2,1)}, bf16[8,512,768]{2,1,0:T(8,128)(2,1)}, bf16[512,1536]{1,0:T(8,128)(2,1)}, bf16[512,1536]{1,0:T(8,128)(2,1)}, bf16[4,512,1536]{2,1,0:T(8,128)(2,1)}) custom-call(bf16[512,1536]{1,0:T(8,128)(2,1)} %get-tuple-element.118.refs_0_.x_ref, ...), custom_call_target="tpu_custom_call", output_to_operand_aliasing={{4}: (6, {})} | custom-call | flops 19327352832 | bytes 50331648 | tf_op jit(solution)/shard_map/mlp_fwd/pallas_call | solution.py:380
  479.2 9.9 norm_kv.6
  495.2 23.6 %attn_fwd.6 = (bf16[4,4,512,1536]{3,2,1,0:T(8,128)(2,1)}, f32[12,2,512]{2,1,0:T(2,128)}) custom-call(bf16[512,1536]{1,0:T(8,128)(2,1)} %convolution_convert_fusion.1.refs_0_.refs_1_.q_ref, bf16[512,1536]{1,0:T(8,128)(2,1)} %convolution_convert_fusion.1.refs_0_.refs_1_.q_ref, ...), custom_call_target="tpu_custom_call", output_to_operand_aliasing={{0}: (8, {})} | custom-call | flops 12884901888 | bytes 9437184 | tf_op jit(solution)/shard_map/attn_fwd/pallas_call | solution.py:114
  518.7 33.7 %mlp_fwd.6 = (bf16[512,6144]{1,0:T(8,128)(2,1)}, bf16[8,512,768]{2,1,0:T(8,128)(2,1)}, bf16[512,1536]{1,0:T(8,128)(2,1)}, bf16[512,1536]{1,0:T(8,128)(2,1)}, bf16[4,512,1536]{2,1,0:T(8,128)(2,1)}) custom-call(bf16[512,1536]{1,0:T(8,128)(2,1)} %get-tuple-element.123.refs_0_.x_ref, ...), custom_call_target="tpu_custom_call", output_to_operand_aliasing={{4}: (6, {})} | custom-call | flops 19327352832 | bytes 50331648 | tf_op jit(solution)/shard_map/mlp_fwd/pallas_call | solution.py:380
  552.4 9.9 norm_kv.7
  573.6 7.7 convolution_convert_fusion.refs_0_.refs_1_.q_ref
  581.4 23.8 %attn_fwd.7 = (bf16[4,4,512,1536]{3,2,1,0:T(8,128)(2,1)}, f32[12,2,512]{2,1,0:T(2,128)}) custom-call(bf16[512,1536]{1,0:T(8,128)(2,1)} %convolution_convert_fusion.refs_0_.refs_1_.q_ref, bf16[512,1536]{1,0:T(8,128)(2,1)} %convolution_convert_fusion.refs_0_.refs_1_.q_ref, ...), custom_call_target="tpu_custom_call", output_to_operand_aliasing={{0}: (8, {})} | custom-call | flops 12884901888 | bytes 9437184 | tf_op jit(solution)/shard_map/attn_fwd/pallas_call | solution.py:114
  605.1 33.6 %mlp_fwd.7 = (bf16[512,6144]{1,0:T(8,128)(2,1)}, bf16[8,512,768]{2,1,0:T(8,128)(2,1)}, bf16[512,1536]{1,0:T(8,128)(2,1)}, bf16[512,1536]{1,0:T(8,128)(2,1)}, bf16[4,512,1536]{2,1,0:T(8,128)(2,1)}) custom-call(bf16[512,1536]{1,0:T(8,128)(2,1)} %get-tuple-element.128.refs_0_.x_ref, ...), custom_call_target="tpu_custom_call", output_to_operand_aliasing={{4}: (6, {})} | custom-call | flops 19327352832 | bytes 50331648 | tf_op jit(solution)/shard_map/mlp_fwd/pallas_call | solution.py:380
  638.8 36.0 %mlp_bwd.4 = (bf16[4,512,6144]{2,1,0:T(8,128)(2,1)}, bf16[2,4,512,1536]{3,2,1,0:T(8,128)(2,1)}, bf16[512,1536]{1,0:T(8,128)(2,1)}) custom-call(bf16[512,1536]{1,0:T(8,128)(2,1)} %bitcast_select_fusion.refs_0_, bf16[512,1536]{1,0:T(8,128)(2,1)} %get-tuple-element.133.refs_1_, ...), custom_call_target="tpu_custom_call", output_to_operand_aliasing={{1}: (6, {})} | custom-call | flops 19327352832 | bytes 50331648 | tf_op jit(solution)/shard_map/mlp_bwd/pallas_call | solution.py:444
  674.7 42.0 %attn_bwd.4 = (bf16[4,4,512,1536]{3,2,1,0:T(8,128)(2,1)}, f32[2,512,1536]{2,1,0:T(8,128)}, f32[2,512,1536]{2,1,0:T(8,128)}) custom-call(bf16[512,1536]{1,0:T(8,128)(2,1)} %convolution_convert_fusion.refs_0_.refs_1_.q_ref, bf16[512,3072]{1,0:T(8,128)(2,1)} %get-tuple-element.130.refs_2_.refs_4_.refs_6_.ko_ref.vo_ref, ...), custom_call_target="tpu_custom_call", output_to_operand_aliasing={{0}: (7, {})} | custom-call | flops 32212254720 | bytes 25165824 | tf_op jit(solution)/shard_map/attn_bwd/pallas_call | solution.py:186
  716.9 6.0 fusion.13.acc0_ref
  727.3 15.8 d_kv.4
  743.2 37.2 %mlp_bwd.5 = (bf16[4,512,6144]{2,1,0:T(8,128)(2,1)}, bf16[2,4,512,1536]{3,2,1,0:T(8,128)(2,1)}, bf16[512,1536]{1,0:T(8,128)(2,1)}) custom-call(bf16[512,1536]{1,0:T(8,128)(2,1)} %get-tuple-element.141.refs_0_, bf16[512,1536]{1,0:T(8,128)(2,1)} %get-tuple-element.142.refs_1_, ...), custom_call_target="tpu_custom_call", output_to_operand_aliasing={{1}: (6, {}), {0}: (7, {})} | custom-call | flops 19327352832 | bytes 50331648 | tf_op jit(solution)/shard_map/mlp_bwd/pallas_call | solution.py:444
  780.3 42.2 %attn_bwd.5 = (bf16[4,4,512,1536]{3,2,1,0:T(8,128)(2,1)}, f32[2,512,1536]{2,1,0:T(8,128)}, f32[2,512,1536]{2,1,0:T(8,128)}) custom-call(bf16[512,1536]{1,0:T(8,128)(2,1)} %convolution_convert_fusion.1.refs_0_.refs_1_.q_ref, bf16[512,3072]{1,0:T(8,128)(2,1)} %get-tuple-element.125.refs_2_.refs_4_.refs_6_.ko_ref.vo_ref, ...), custom_call_target="tpu_custom_call", output_to_operand_aliasing={{0}: (7, {})} | custom-call | flops 32212254720 | bytes 25165824 | tf_op jit(solution)/shard_map/attn_bwd/pallas_call | solution.py:186
  822.6 6.0 fusion.11.acc0_ref
  833.0 15.8 d_kv.5
  848.8 37.4 %mlp_bwd.6 = (bf16[4,512,6144]{2,1,0:T(8,128)(2,1)}, bf16[2,4,512,1536]{3,2,1,0:T(8,128)(2,1)}, bf16[512,1536]{1,0:T(8,128)(2,1)}) custom-call(bf16[512,1536]{1,0:T(8,128)(2,1)} %get-tuple-element.152.refs_0_, bf16[512,1536]{1,0:T(8,128)(2,1)} %get-tuple-element.153.refs_1_, ...), custom_call_target="tpu_custom_call", output_to_operand_aliasing={{1}: (6, {}), {0}: (7, {})} | custom-call | flops 19327352832 | bytes 50331648 | tf_op jit(solution)/shard_map/mlp_bwd/pallas_call | solution.py:444
  886.3 42.1 %attn_bwd.6 = (bf16[4,4,512,1536]{3,2,1,0:T(8,128)(2,1)}, f32[2,512,1536]{2,1,0:T(8,128)}, f32[2,512,1536]{2,1,0:T(8,128)}) custom-call(bf16[512,1536]{1,0:T(8,128)(2,1)} %convolution_convert_fusion.2.refs_0_.refs_1_.q_ref, bf16[512,3072]{1,0:T(8,128)(2,1)} %get-tuple-element.120.refs_2_.refs_4_.refs_6_.ko_ref.vo_ref, ...), custom_call_target="tpu_custom_call", output_to_operand_aliasing={{0}: (7, {})} | custom-call | flops 32212254720 | bytes 25165824 | tf_op jit(solution)/shard_map/attn_bwd/pallas_call | solution.py:186
  929.1 6.0 fusion.9.acc0_ref
  938.9 15.8 d_kv.6
  954.7 36.1 %mlp_bwd.7 = (bf16[4,512,6144]{2,1,0:T(8,128)(2,1)}, bf16[2,4,512,1536]{3,2,1,0:T(8,128)(2,1)}, bf16[512,1536]{1,0:T(8,128)(2,1)}) custom-call(bf16[512,1536]{1,0:T(8,128)(2,1)} %get-tuple-element.163.refs_0_, bf16[512,1536]{1,0:T(8,128)(2,1)} %get-tuple-element.164.refs_1_, ...), custom_call_target="tpu_custom_call", output_to_operand_aliasing={{1}: (6, {}), {0}: (7, {})} | custom-call | flops 19327352832 | bytes 50331648 | tf_op jit(solution)/shard_map/mlp_bwd/pallas_call | solution.py:444
  990.8 21.4 %shard_map.146 = (f32[2,384,768]{2,1,0:T(8,128)}, f32[2,384,768]{2,1,0:T(8,128)}, f32[2,384,768]{2,1,0:T(8,128)}, f32[2,384,768]{2,1,0:T(8,128)}) custom-call(s32[5]{0:T(128)} %stack.32.places_ref, bf16[1,2048,6144]{2,1,0:T(8,128)(2,1)} %bitcast.75, bf16[1,2048,1536]{2,1,0:T(8,128)(2,1)} %bitcast.79), custom_call_target="tpu_custom_call" | custom-call | flops 9663676416 | bytes 18874368 | tf_op jit(solution)/shard_map/pallas_call | solution.py:296
  1013.3 21.5 %shard_map.144 = (f32[2,384,768]{2,1,0:T(8,128)}, f32[2,384,768]{2,1,0:T(8,128)}, f32[2,384,768]{2,1,0:T(8,128)}, f32[2,384,768]{2,1,0:T(8,128)}) custom-call(s32[5]{0:T(128)} %stack.32.places_ref, bf16[1,2048,6144]{2,1,0:T(8,128)(2,1)} %bitcast.76, bf16[1,2048,1536]{2,1,0:T(8,128)(2,1)} %bitcast.80), custom_call_target="tpu_custom_call" | custom-call | flops 9663676416 | bytes 18874368 | tf_op jit(solution)/shard_map/pallas_call | solution.py:296
  1040.5 24.0 %shard_map.147 = (f32[2,384,768]{2,1,0:T(8,128)}, f32[2,384,768]{2,1,0:T(8,128)}, f32[2,384,768]{2,1,0:T(8,128)}, f32[2,384,768]{2,1,0:T(8,128)}) custom-call(s32[5]{0:T(128)} %stack.30.places_ref, bf16[1,2048,6144]{2,1,0:T(8,128)(2,1)} %bitcast.77, bf16[1,2048,1536]{2,1,0:T(8,128)(2,1)} %bitcast.81, f32[2,384,768]{2,1,0:T(8,128)} %collective-permute-done.37.refs_0_, ...), custom_call_target="tpu_custom_call" | custom-call | flops 9663676416 | bytes 18874368 | tf_op jit(solution)/shard_map/pallas_call | solution.py:296
  1065.9 22.9 %shard_map.145 = (f32[2,384,768]{2,1,0:T(8,128)}, f32[2,384,768]{2,1,0:T(8,128)}, f32[2,384,768]{2,1,0:T(8,128)}, f32[2,384,768]{2,1,0:T(8,128)}) custom-call(s32[5]{0:T(128)} %stack.30.places_ref, bf16[1,2048,6144]{2,1,0:T(8,128)(2,1)} %bitcast.78, bf16[1,2048,1536]{2,1,0:T(8,128)(2,1)} %bitcast.82, f32[2,384,768]{2,1,0:T(8,128)} %copy-done.13, ...), custom_call_target="tpu_custom_call" | custom-call | flops 9663676416 | bytes 18874368 | tf_op jit(solution)/shard_map/pallas_call | solution.py:296
  1088.8 41.8 %attn_bwd.7 = (bf16[4,4,512,1536]{3,2,1,0:T(8,128)(2,1)}, f32[2,512,1536]{2,1,0:T(8,128)}, f32[2,512,1536]{2,1,0:T(8,128)}) custom-call(bf16[512,1536]{1,0:T(8,128)(2,1)} %convolution_convert_fusion.3.refs_0_.refs_1_.q_ref, bf16[512,3072]{1,0:T(8,128)(2,1)} %get-tuple-element.116.refs_2_.refs_4_.refs_6_.ko_ref.vo_ref, ...), custom_call_target="tpu_custom_call", output_to_operand_aliasing={{0}: (7, {})} | custom-call | flops 32212254720 | bytes 25165824 | tf_op jit(solution)/shard_map/attn_bwd/pallas_call | solution.py:186
  1131.1 9.6 all-to-all-done.1
  1148.5 131.5 %collective-permute-done.62 = f32[2,384,768]{2,1,0:T(8,128)S(1)} collective-permute-done((f32[2,384,768]{2,1,0:T(8,128)}, f32[2,384,768]{2,1,0:T(8,128)S(1)}, u32[]{:S(2)}, u32[]{:S(2)}) %collective-permute-start.62) | collective-permute-done | bytes 2359328 | tf_op jit(solution)/shard_map/ppermute | solution.py:31
  1287.7 15.8 d_kv.7
  1303.5 20.4 %shard_map.150 = (f32[2,384,768]{2,1,0:T(8,128)}, f32[2,384,768]{2,1,0:T(8,128)}, f32[2,384,768]{2,1,0:T(8,128)}, f32[2,384,768]{2,1,0:T(8,128)}) custom-call(s32[5]{0:T(128)} %stack.32.places_ref, bf16[4,2048,1536]{2,1,0:T(8,128)(2,1)} %bitcast.67, bf16[2,2048,1536]{2,1,0:T(8,128)(2,1)} %bitcast.71), custom_call_target="tpu_custom_call" | custom-call | flops 9663676416 | bytes 18874368 | tf_op jit(solution)/shard_map/pallas_call | solution.py:296
  1324.4 6.1 collective-permute-done.61
  1335.0 20.3 %shard_map.148 = (f32[2,384,768]{2,1,0:T(8,128)}, f32[2,384,768]{2,1,0:T(8,128)}, f32[2,384,768]{2,1,0:T(8,128)}, f32[2,384,768]{2,1,0:T(8,128)}) custom-call(s32[5]{0:T(128)} %stack.32.places_ref, bf16[4,2048,1536]{2,1,0:T(8,128)(2,1)} %bitcast.68, bf16[2,2048,1536]{2,1,0:T(8,128)(2,1)} %bitcast.72), custom_call_target="tpu_custom_call" | custom-call | flops 9663676416 | bytes 18874368 | tf_op jit(solution)/shard_map/pallas_call | solution.py:296
  1370.2 22.3 %shard_map.151 = (f32[2,384,768]{2,1,0:T(8,128)}, f32[2,384,768]{2,1,0:T(8,128)}, f32[2,384,768]{2,1,0:T(8,128)}, f32[2,384,768]{2,1,0:T(8,128)}) custom-call(s32[5]{0:T(128)} %stack.30.places_ref, bf16[4,2048,1536]{2,1,0:T(8,128)(2,1)} %bitcast.69, bf16[2,2048,1536]{2,1,0:T(8,128)(2,1)} %bitcast.73, f32[2,384,768]{2,1,0:T(8,128)} %copy-done.5, ...), custom_call_target="tpu_custom_call" | custom-call | flops 9663676416 | bytes 18874368 | tf_op jit(solution)/shard_map/pallas_call | solution.py:296
  1396.6 22.3 %shard_map.149 = (f32[2,384,768]{2,1,0:T(8,128)}, f32[2,384,768]{2,1,0:T(8,128)}, f32[2,384,768]{2,1,0:T(8,128)}, f32[2,384,768]{2,1,0:T(8,128)}) custom-call(s32[5]{0:T(128)} %stack.30.places_ref, bf16[4,2048,1536]{2,1,0:T(8,128)(2,1)} %bitcast.70, bf16[2,2048,1536]{2,1,0:T(8,128)(2,1)} %bitcast.74, f32[2,384,768]{2,1,0:T(8,128)} %collective-permute-done.42.refs_0_, ...), custom_call_target="tpu_custom_call" | custom-call | flops 9663676416 | bytes 18874368 | tf_op jit(solution)/shard_map/pallas_call | solution.py:296
  1422.7 16.3 fusion.31
  1439.0 10.0 fusion.2
  1451.0 10.0 fusion
  1461.0 113.6 %all-to-all-done.2 = bf16[8,512,768]{2,1,0:T(8,128)(2,1)} async-done(((bf16[8,512,768]{2,1,0:T(8,128)(2,1)}), bf16[8,512,768]{2,1,0:T(8,128)(2,1)}, u32[]{:S(2)}, u32[]{:S(2)}) %all-to-all-start.2) | async-done | bytes 6291488 | tf_op jit(solution)/shard_map/all_to_all | solution.py:611
  1586.4 16.7 fusion.32
  1605.2 19.9 %collective-permute-done.53 = f32[2,384,768]{2,1,0:T(8,128)} collective-permute-done((f32[2,384,768]{2,1,0:T(8,128)}, f32[2,384,768]{2,1,0:T(8,128)}, u32[]{:S(2)}, u32[]{:S(2)}) %collective-permute-start.53) | collective-permute-done | bytes 2359328 | tf_op jit(solution)/shard_map/ppermute | solution.py:31
  1625.5 21.7 %add_add_fusion.refs_0_ = f32[768,1536]{1,0:T(8,128)} fusion(f32[768,1536]{1,0:T(8,128)} %fusion.32, f32[768,1536]{1,0:T(8,128)} %fusion.31, f32[768,1536]{1,0:T(8,128)} %fusion.2, f32[768,1536]{1,0:T(8,128)} %fusion, bf16[4096,768]{1,0:T(8,128)(2,1)} %bitcast.31, bf16[4096,1536]{1,0:T(8,128)(2,1)} %all-gather.14.cloned.1.call-done), kind=kOutput, calls=%fused_computation.3 | convolution fusion | flops 9668395008 | bytes 42467328 | tf_op jit(solution)/shard_map/dot_general | solution.py:39
  1647.1 34.8 %collective-permute-done.69 = bf16[1024,1536]{1,0:T(8,128)(2,1)} collective-permute-done((bf16[1024,1536]{1,0:T(8,128)(2,1)}, bf16[1024,1536]{1,0:T(8,128)(2,1)}, u32[]{:S(2)}, u32[]{:S(2)}) %collective-permute-start.69) | collective-permute-done | bytes 3145760 | tf_op jit(solution)/shard_map/ppermute | solution.py:650
  1689.7 6.0 add_add_fusion.2
  1695.7 12.4 collective-permute-done.55
  1717.3 8.9 shard_map.153
  1726.2 45.8 %collective-permute-done.70 = bf16[1024,1536]{1,0:T(8,128)(2,1)} collective-permute-done((bf16[1024,1536]{1,0:T(8,128)(2,1)}, bf16[1024,1536]{1,0:T(8,128)(2,1)}, u32[]{:S(2)}, u32[]{:S(2)}) %collective-permute-start.70) | collective-permute-done | bytes 3145760 | tf_op jit(solution)/shard_map/ppermute | solution.py:27
  1777.2 8.4 shard_map.152
  1785.6 11.6 shard_map.154
  (281 shorter events, 239.4 us)
Async XLA Ops:
  7.2 288.2 %all-gather.6.cloned.1.call-start = ((), (), s32[]{:S(2)}) async-start(), calls=%async_computation.4 | async-start | bytes 15925248 | tf_op jit(solution)/shard_map/all_gather | solution.py:567
  16.1 319.2 %all-gather.8.cloned.1.call-start = ((), (), s32[]{:S(2)}) async-start(), calls=%async_computation.5 | async-start | bytes 5308416 | tf_op jit(solution)/shard_map/all_gather | solution.py:567
  26.5 50.1 %collective-permute-start.2 = (bf16[384,1536]{1,0:T(8,128)(2,1)}, bf16[384,1536]{1,0:T(8,128)(2,1)}, u32[]{:S(2)}, u32[]{:S(2)}) collective-permute-start(bf16[384,1536]{1,0:T(8,128)(2,1)} %get-tuple-element.237), channel_id=1, source_target_pairs={{0,2},{2,0},{4,6},{6,4},{1,3},{3,1},{5,7},{7,5}} | collective-permute-start | bytes 3538952 | tf_op jit(solution)/shard_map/ppermute | solution.py:27
  29.9 100.3 %collective-permute-start.6 = (bf16[384,1536]{1,0:T(8,128)(2,1)}, bf16[384,1536]{1,0:T(8,128)(2,1)}, u32[]{:S(2)}, u32[]{:S(2)}) collective-permute-start(bf16[384,1536]{1,0:T(8,128)(2,1)} %get-tuple-element.237), channel_id=1, source_target_pairs={{0,4},{4,0},{2,6},{6,2},{1,5},{5,1},{3,7},{7,3}} | collective-permute-start | bytes 3538952 | tf_op jit(solution)/shard_map/ppermute | solution.py:31
  31.4 95.8 %collective-permute-start.4 = (bf16[384,1536]{1,0:T(8,128)(2,1)}, bf16[384,1536]{1,0:T(8,128)(2,1)}, u32[]{:S(2)}, u32[]{:S(2)}) collective-permute-start(bf16[384,1536]{1,0:T(8,128)(2,1)} %get-tuple-element.236), channel_id=1, source_target_pairs={{0,2},{2,0},{4,6},{6,4},{1,3},{3,1},{5,7},{7,5}} | collective-permute-start | bytes 3538952 | tf_op jit(solution)/shard_map/ppermute | solution.py:27
  35.1 131.0 %collective-permute-start.14 = (bf16[384,1536]{1,0:T(8,128)(2,1)}, bf16[384,1536]{1,0:T(8,128)(2,1)}, u32[]{:S(2)}, u32[]{:S(2)}) collective-permute-start(bf16[384,1536]{1,0:T(8,128)(2,1)} %get-tuple-element.231), channel_id=1, source_target_pairs={{0,2},{2,0},{4,6},{6,4},{1,3},{3,1},{5,7},{7,5}} | collective-permute-start | bytes 3538952 | tf_op jit(solution)/shard_map/ppermute | solution.py:27
  38.3 129.3 %collective-permute-start = (bf16[512,1536]{1,0:T(8,128)(2,1)S(1)}, bf16[512,1536]{1,0:T(8,128)(2,1)}, u32[]{:S(2)}, u32[]{:S(2)}) collective-permute-start(bf16[512,1536]{1,0:T(8,128)(2,1)S(1)} %dynamic-slice_bitcast_fusion.2), channel_id=1, source_target_pairs={{0,1},{1,0},{2,3},{3,2},{4,5},{5,4},{6,7},{7,6}} | collective-permute-start | bytes 4718600 | tf_op jit(solution)/shard_map/ppermute | solution.py:35
  39.3 1383.4 %all-gather.10.cloned.1.call-start = ((), (), s32[]{:S(2)}) async-start(), calls=%async_computation.6 | async-start | bytes 14155776 | tf_op jit(solution)/shard_map/all_gather | solution.py:567
  76.6 93.4 %collective-permute-start.3 = (bf16[384,1536]{1,0:T(8,128)(2,1)}, bf16[384,1536]{1,0:T(8,128)(2,1)S(1)}, u32[]{:S(2)}, u32[]{:S(2)}) collective-permute-start(bf16[384,1536]{1,0:T(8,128)(2,1)} %collective-permute-done.2), channel_id=1, source_target_pairs={{0,1},{1,0},{2,3},{3,2},{4,5},{5,4},{6,7},{7,6}} | collective-permute-start | bytes 3538952 | tf_op jit(solution)/shard_map/ppermute | solution.py:35
  127.2 78.0 %collective-permute-start.16 = (bf16[384,1536]{1,0:T(8,128)(2,1)S(1)}, bf16[384,1536]{1,0:T(8,128)(2,1)S(1)}, u32[]{:S(2)}, u32[]{:S(2)}) collective-permute-start(bf16[384,1536]{1,0:T(8,128)(2,1)S(1)} %copy-done.25), channel_id=1, source_target_pairs={{0,2},{2,0},{4,6},{6,4},{1,3},{3,1},{5,7},{7,5}} | collective-permute-start | bytes 3538952 | tf_op jit(solution)/shard_map/ppermute | solution.py:27
  130.2 77.6 %collective-permute-start.8 = (bf16[384,1536]{1,0:T(8,128)(2,1)}, bf16[384,1536]{1,0:T(8,128)(2,1)S(1)}, u32[]{:S(2)}, u32[]{:S(2)}) collective-permute-start(bf16[384,1536]{1,0:T(8,128)(2,1)} %get-tuple-element.236), channel_id=1, source_target_pairs={{0,4},{4,0},{2,6},{6,2},{1,5},{5,1},{3,7},{7,3}} | collective-permute-start | bytes 3538952 | tf_op jit(solution)/shard_map/ppermute | solution.py:31
  166.1 43.2 %collective-permute-start.18 = (bf16[384,1536]{1,0:T(8,128)(2,1)}, bf16[384,1536]{1,0:T(8,128)(2,1)S(1)}, u32[]{:S(2)}, u32[]{:S(2)}) collective-permute-start(bf16[384,1536]{1,0:T(8,128)(2,1)} %get-tuple-element.231), channel_id=1, source_target_pairs={{0,4},{4,0},{2,6},{6,2},{1,5},{5,1},{3,7},{7,3}} | collective-permute-start | bytes 3538952 | tf_op jit(solution)/shard_map/ppermute | solution.py:31
  167.7 41.7 %collective-permute-start.15 = (bf16[384,1536]{1,0:T(8,128)(2,1)}, bf16[384,1536]{1,0:T(8,128)(2,1)S(1)}, u32[]{:S(2)}, u32[]{:S(2)}) collective-permute-start(bf16[384,1536]{1,0:T(8,128)(2,1)} %collective-permute-done.14), channel_id=1, source_target_pairs={{0,1},{1,0},{2,3},{3,2},{4,5},{5,4},{6,7},{7,6}} | collective-permute-start | bytes 3538952 | tf_op jit(solution)/shard_map/ppermute | solution.py:35
  170.0 42.0 %collective-permute-start.5 = (bf16[384,1536]{1,0:T(8,128)(2,1)}, bf16[384,1536]{1,0:T(8,128)(2,1)S(1)}, u32[]{:S(2)}, u32[]{:S(2)}) collective-permute-start(bf16[384,1536]{1,0:T(8,128)(2,1)} %collective-permute-done.4), channel_id=1, source_target_pairs={{0,1},{1,0},{2,3},{3,2},{4,5},{5,4},{6,7},{7,6}} | collective-permute-start | bytes 3538952 | tf_op jit(solution)/shard_map/ppermute | solution.py:35
  207.8 28.8 %collective-permute-start.20 = (bf16[384,1536]{1,0:T(8,128)(2,1)S(1)}, bf16[384,1536]{1,0:T(8,128)(2,1)S(1)}, u32[]{:S(2)}, u32[]{:S(2)}) collective-permute-start(bf16[384,1536]{1,0:T(8,128)(2,1)S(1)} %copy-done.25), channel_id=1, source_target_pairs={{0,4},{4,0},{2,6},{6,2},{1,5},{5,1},{3,7},{7,3}} | collective-permute-start | bytes 3538952 | tf_op jit(solution)/shard_map/ppermute | solution.py:31
  209.3 27.7 %collective-permute-start.7 = (bf16[384,1536]{1,0:T(8,128)(2,1)}, bf16[384,1536]{1,0:T(8,128)(2,1)S(1)}, u32[]{:S(2)}, u32[]{:S(2)}) collective-permute-start(bf16[384,1536]{1,0:T(8,128)(2,1)} %collective-permute-done.6), channel_id=1, source_target_pairs={{0,1},{1,0},{2,3},{3,2},{4,5},{5,4},{6,7},{7,6}} | collective-permute-start | bytes 3538952 | tf_op jit(solution)/shard_map/ppermute | solution.py:35
  209.3 29.3 %collective-permute-start.9 = (bf16[384,1536]{1,0:T(8,128)(2,1)S(1)}, bf16[384,1536]{1,0:T(8,128)(2,1)S(1)}, u32[]{:S(2)}, u32[]{:S(2)}) collective-permute-start(bf16[384,1536]{1,0:T(8,128)(2,1)S(1)} %collective-permute-done.8), channel_id=1, source_target_pairs={{0,1},{1,0},{2,3},{3,2},{4,5},{5,4},{6,7},{7,6}} | collective-permute-start | bytes 3538952 | tf_op jit(solution)/shard_map/ppermute | solution.py:35
  212.0 30.3 %collective-permute-start.19 = (bf16[384,1536]{1,0:T(8,128)(2,1)S(1)}, bf16[384,1536]{1,0:T(8,128)(2,1)S(1)}, u32[]{:S(2)}, u32[]{:S(2)}) collective-permute-start(bf16[384,1536]{1,0:T(8,128)(2,1)S(1)} %collective-permute-done.18), channel_id=1, source_target_pairs={{0,1},{1,0},{2,3},{3,2},{4,5},{5,4},{6,7},{7,6}} | collective-permute-start | bytes 3538952 | tf_op jit(solution)/shard_map/ppermute | solution.py:35
  215.6 46.3 %collective-permute-start.10 = (bf16[384,1536]{1,0:T(8,128)(2,1)}, bf16[384,1536]{1,0:T(8,128)(2,1)S(1)}, u32[]{:S(2)}, u32[]{:S(2)}) collective-permute-start(bf16[384,1536]{1,0:T(8,128)(2,1)} %collective-permute-done.2), channel_id=1, source_target_pairs={{0,4},{4,0},{2,6},{6,2},{1,5},{5,1},{3,7},{7,3}} | collective-permute-start | bytes 3538952 | tf_op jit(solution)/shard_map/ppermute | solution.py:31
  236.6 28.8 %collective-permute-start.12 = (bf16[384,1536]{1,0:T(8,128)(2,1)S(1)}, bf16[384,1536]{1,0:T(8,128)(2,1)S(1)}, u32[]{:S(2)}, u32[]{:S(2)}) collective-permute-start(bf16[384,1536]{1,0:T(8,128)(2,1)S(1)} %collective-permute-done.8), channel_id=1, source_target_pairs={{0,2},{2,0},{4,6},{6,4},{1,3},{3,1},{5,7},{7,5}} | collective-permute-start | bytes 3538952 | tf_op jit(solution)/shard_map/ppermute | solution.py:27
  237.0 49.6 %collective-permute-start.22 = (bf16[384,1536]{1,0:T(8,128)(2,1)}, bf16[384,1536]{1,0:T(8,128)(2,1)}, u32[]{:S(2)}, u32[]{:S(2)}) collective-permute-start(bf16[384,1536]{1,0:T(8,128)(2,1)} %collective-permute-done.14), channel_id=1, source_target_pairs={{0,4},{4,0},{2,6},{6,2},{1,5},{5,1},{3,7},{7,3}} | collective-permute-start | bytes 3538952 | tf_op jit(solution)/shard_map/ppermute | solution.py:31
  238.7 49.9 %collective-permute-start.24 = (bf16[384,1536]{1,0:T(8,128)(2,1)S(1)}, bf16[384,1536]{1,0:T(8,128)(2,1)}, u32[]{:S(2)}, u32[]{:S(2)}) collective-permute-start(bf16[384,1536]{1,0:T(8,128)(2,1)S(1)} %collective-permute-done.20), channel_id=1, source_target_pairs={{0,2},{2,0},{4,6},{6,4},{1,3},{3,1},{5,7},{7,5}} | collective-permute-start | bytes 3538952 | tf_op jit(solution)/shard_map/ppermute | solution.py:27
  242.3 48.5 %collective-permute-start.21 = (bf16[384,1536]{1,0:T(8,128)(2,1)S(1)}, bf16[384,1536]{1,0:T(8,128)(2,1)S(1)}, u32[]{:S(2)}, u32[]{:S(2)}) collective-permute-start(bf16[384,1536]{1,0:T(8,128)(2,1)S(1)} %collective-permute-done.20), channel_id=1, source_target_pairs={{0,1},{1,0},{2,3},{3,2},{4,5},{5,4},{6,7},{7,6}} | collective-permute-start | bytes 3538952 | tf_op jit(solution)/shard_map/ppermute | solution.py:35
  261.9 32.5 %collective-permute-start.11 = (bf16[384,1536]{1,0:T(8,128)(2,1)S(1)}, bf16[384,1536]{1,0:T(8,128)(2,1)S(1)}, u32[]{:S(2)}, u32[]{:S(2)}) collective-permute-start(bf16[384,1536]{1,0:T(8,128)(2,1)S(1)} %collective-permute-done.10), channel_id=1, source_target_pairs={{0,1},{1,0},{2,3},{3,2},{4,5},{5,4},{6,7},{7,6}} | collective-permute-start | bytes 3538952 | tf_op jit(solution)/shard_map/ppermute | solution.py:35
  265.4 65.1 %collective-permute-start.13 = (bf16[384,1536]{1,0:T(8,128)(2,1)S(1)}, bf16[384,1536]{1,0:T(8,128)(2,1)}, u32[]{:S(2)}, u32[]{:S(2)}) collective-permute-start(bf16[384,1536]{1,0:T(8,128)(2,1)S(1)} %collective-permute-done.12), channel_id=1, source_target_pairs={{0,1},{1,0},{2,3},{3,2},{4,5},{5,4},{6,7},{7,6}} | collective-permute-start | bytes 3538952 | tf_op jit(solution)/shard_map/ppermute | solution.py:35
  286.6 39.2 %collective-permute-start.23 = (bf16[384,1536]{1,0:T(8,128)(2,1)}, bf16[384,1536]{1,0:T(8,128)(2,1)}, u32[]{:S(2)}, u32[]{:S(2)}) collective-permute-start(bf16[384,1536]{1,0:T(8,128)(2,1)} %collective-permute-done.22), channel_id=1, source_target_pairs={{0,1},{1,0},{2,3},{3,2},{4,5},{5,4},{6,7},{7,6}} | collective-permute-start | bytes 3538952 | tf_op jit(solution)/shard_map/ppermute | solution.py:35
  288.6 44.3 %collective-permute-start.25 = (bf16[384,1536]{1,0:T(8,128)(2,1)}, bf16[384,1536]{1,0:T(8,128)(2,1)}, u32[]{:S(2)}, u32[]{:S(2)}) collective-permute-start(bf16[384,1536]{1,0:T(8,128)(2,1)} %collective-permute-done.24), channel_id=1, source_target_pairs={{0,1},{1,0},{2,3},{3,2},{4,5},{5,4},{6,7},{7,6}} | collective-permute-start | bytes 3538952 | tf_op jit(solution)/shard_map/ppermute | solution.py:35
  743.1 843.3 %all-gather.12.cloned.1.call-start = ((), (), s32[]{:S(2)}) async-start(), calls=%async_computation.7 | async-start | bytes 14155776 | tf_op jit(solution)/shard_map/all_gather | solution.py:567
  1034.8 29.7 %collective-permute-start.33 = (f32[2,384,768]{2,1,0:T(8,128)}, f32[2,384,768]{2,1,0:T(8,128)S(1)}, u32[]{:S(2)}, u32[]{:S(2)}) collective-permute-start(f32[2,384,768]{2,1,0:T(8,128)} %get-tuple-element.170), channel_id=1, source_target_pairs={{0,1},{1,0},{2,3},{3,2},{4,5},{5,4},{6,7},{7,6}} | collective-permute-start | bytes 7077896 | tf_op jit(solution)/shard_map/ppermute | solution.py:35
  1034.9 29.6 %collective-permute-start.34 = (f32[2,384,768]{2,1,0:T(8,128)}, f32[2,384,768]{2,1,0:T(8,128)}, u32[]{:S(2)}, u32[]{:S(2)}) collective-permute-start(f32[2,384,768]{2,1,0:T(8,128)} %get-tuple-element.171), channel_id=1, source_target_pairs={{0,1},{1,0},{2,3},{3,2},{4,5},{5,4},{6,7},{7,6}} | collective-permute-start | bytes 7077896 | tf_op jit(solution)/shard_map/ppermute | solution.py:35
  1035.3 29.3 %collective-permute-start.35 = (f32[2,384,768]{2,1,0:T(8,128)}, f32[2,384,768]{2,1,0:T(8,128)}, u32[]{:S(2)}, u32[]{:S(2)}) collective-permute-start(f32[2,384,768]{2,1,0:T(8,128)} %get-tuple-element.172), channel_id=1, source_target_pairs={{0,1},{1,0},{2,3},{3,2},{4,5},{5,4},{6,7},{7,6}} | collective-permute-start | bytes 7077896 | tf_op jit(solution)/shard_map/ppermute | solution.py:35
  1035.4 29.1 %collective-permute-start.36 = (f32[2,384,768]{2,1,0:T(8,128)}, f32[2,384,768]{2,1,0:T(8,128)}, u32[]{:S(2)}, u32[]{:S(2)}) collective-permute-start(f32[2,384,768]{2,1,0:T(8,128)} %get-tuple-element.173), channel_id=1, source_target_pairs={{0,1},{1,0},{2,3},{3,2},{4,5},{5,4},{6,7},{7,6}} | collective-permute-start | bytes 7077896 | tf_op jit(solution)/shard_map/ppermute | solution.py:35
  1036.4 104.2 %all-to-all-start.1 = ((bf16[8,512,768]{2,1,0:T(8,128)(2,1)}), bf16[8,512,768]{2,1,0:T(8,128)(2,1)}, u32[]{:S(2)}, u32[]{:S(2)}) async-start(bf16[8,512,768]{2,1,0:T(8,128)(2,1)} %get-tuple-element.216), calls=%async_computation.1 | async-start | bytes 12582912 | tf_op jit(solution)/shard_map/all_to_all | solution.py:611
  1039.9 585.5 %all-gather.14.cloned.1.call-start = ((), (), s32[]{:S(2)}) async-start(), calls=%async_computation.8 | async-start | bytes 14155776 | tf_op jit(solution)/shard_map/all_gather | solution.py:567
  1130.7 157.0 %collective-permute-start.41 = (f32[2,512,1536]{2,1,0:T(8,128)}, f32[2,512,1536]{2,1,0:T(8,128)}, u32[]{:S(2)}, u32[]{:S(2)}) collective-permute-start(f32[2,512,1536]{2,1,0:T(8,128)} %get-tuple-element.190), channel_id=1, source_target_pairs={{0,1},{1,0},{2,3},{3,2},{4,5},{5,4},{6,7},{7,6}} | collective-permute-start | bytes 18874376 | tf_op jit(solution)/shard_map/ppermute | solution.py:35
  1140.7 189.9 %all-to-all-start = ((bf16[8,512,768]{2,1,0:T(8,128)(2,1)}), bf16[8,512,768]{2,1,0:T(8,128)(2,1)}, u32[]{:S(2)}, u32[]{:S(2)}) async-start(bf16[8,512,768]{2,1,0:T(8,128)(2,1)} %get-tuple-element.214), calls=%async_computation | async-start | bytes 12582912 | tf_op jit(solution)/shard_map/all_to_all | solution.py:611
  1144.5 135.5 %collective-permute-start.62 = (f32[2,384,768]{2,1,0:T(8,128)}, f32[2,384,768]{2,1,0:T(8,128)S(1)}, u32[]{:S(2)}, u32[]{:S(2)}) collective-permute-start(f32[2,384,768]{2,1,0:T(8,128)} %get-tuple-element.183), channel_id=1, source_target_pairs={{0,4},{4,0},{2,6},{6,2},{1,5},{5,1},{3,7},{7,3}} | collective-permute-start | bytes 7077896 | tf_op jit(solution)/shard_map/ppermute | solution.py:31
  1146.5 184.0 %collective-permute-start.61 = (f32[2,384,768]{2,1,0:T(8,128)}, f32[2,384,768]{2,1,0:T(8,128)}, u32[]{:S(2)}, u32[]{:S(2)}) collective-permute-start(f32[2,384,768]{2,1,0:T(8,128)} %get-tuple-element.181), channel_id=1, source_target_pairs={{0,4},{4,0},{2,6},{6,2},{1,5},{5,1},{3,7},{7,3}} | collective-permute-start | bytes 7077896 | tf_op jit(solution)/shard_map/ppermute | solution.py:31
  1146.6 187.7 %collective-permute-start.59 = (f32[2,384,768]{2,1,0:T(8,128)}, f32[2,384,768]{2,1,0:T(8,128)}, u32[]{:S(2)}, u32[]{:S(2)}) collective-permute-start(f32[2,384,768]{2,1,0:T(8,128)} %get-tuple-element.182), channel_id=1, source_target_pairs={{0,2},{2,0},{4,6},{6,4},{1,3},{3,1},{5,7},{7,5}} | collective-permute-start | bytes 7077896 | tf_op jit(solution)/shard_map/ppermute | solution.py:27
  1281.7 53.3 %collective-permute-start.63 = (f32[2,384,768]{2,1,0:T(8,128)}, f32[2,384,768]{2,1,0:T(8,128)}, u32[]{:S(2)}, u32[]{:S(2)}) collective-permute-start(f32[2,384,768]{2,1,0:T(8,128)} %add.357), channel_id=1, source_target_pairs={{0,2},{2,0},{4,6},{6,4},{1,3},{3,1},{5,7},{7,5}} | collective-permute-start | bytes 7077896 | tf_op jit(solution)/shard_map/ppermute | solution.py:27
  1323.9 32.0 %collective-permute-start.46 = (f32[2,384,768]{2,1,0:T(8,128)}, f32[2,384,768]{2,1,0:T(8,128)S(1)}, u32[]{:S(2)}, u32[]{:S(2)}) collective-permute-start(f32[2,384,768]{2,1,0:T(8,128)} %get-tuple-element.197), channel_id=1, source_target_pairs={{0,1},{1,0},{2,3},{3,2},{4,5},{5,4},{6,7},{7,6}} | collective-permute-start | bytes 7077896 | tf_op jit(solution)/shard_map/ppermute | solution.py:35
  1323.9 32.0 %collective-permute-start.47 = (f32[2,384,768]{2,1,0:T(8,128)}, f32[2,384,768]{2,1,0:T(8,128)}, u32[]{:S(2)}, u32[]{:S(2)}) collective-permute-start(f32[2,384,768]{2,1,0:T(8,128)} %get-tuple-element.198), channel_id=1, source_target_pairs={{0,1},{1,0},{2,3},{3,2},{4,5},{5,4},{6,7},{7,6}} | collective-permute-start | bytes 7077896 | tf_op jit(solution)/shard_map/ppermute | solution.py:35
  1330.5 88.4 %all-to-all-start.3 = ((bf16[8,512,768]{2,1,0:T(8,128)(2,1)}), bf16[8,512,768]{2,1,0:T(8,128)(2,1)}, u32[]{:S(2)}, u32[]{:S(2)}) async-start(bf16[8,512,768]{2,1,0:T(8,128)(2,1)} %get-tuple-element.220), calls=%async_computation.3 | async-start | bytes 12582912 | tf_op jit(solution)/shard_map/all_to_all | solution.py:611
  1335.0 28.8 %collective-permute-start.49 = (f32[2,384,768]{2,1,0:T(8,128)}, f32[2,384,768]{2,1,0:T(8,128)}, u32[]{:S(2)}, u32[]{:S(2)}) collective-permute-start(f32[2,384,768]{2,1,0:T(8,128)} %get-tuple-element.200), channel_id=1, source_target_pairs={{0,1},{1,0},{2,3},{3,2},{4,5},{5,4},{6,7},{7,6}} | collective-permute-start | bytes 7077896 | tf_op jit(solution)/shard_map/ppermute | solution.py:35
  1355.3 37.2 %collective-permute-start.42 = (f32[2,384,768]{2,1,0:T(8,128)}, f32[2,384,768]{2,1,0:T(8,128)}, u32[]{:S(2)}, u32[]{:S(2)}) collective-permute-start(f32[2,384,768]{2,1,0:T(8,128)} %get-tuple-element.192), channel_id=1, source_target_pairs={{0,1},{1,0},{2,3},{3,2},{4,5},{5,4},{6,7},{7,6}} | collective-permute-start | bytes 7077896 | tf_op jit(solution)/shard_map/ppermute | solution.py:35
  1355.9 38.1 %collective-permute-start.43 = (f32[2,384,768]{2,1,0:T(8,128)}, f32[2,384,768]{2,1,0:T(8,128)}, u32[]{:S(2)}, u32[]{:S(2)}) collective-permute-start(f32[2,384,768]{2,1,0:T(8,128)} %get-tuple-element.193), channel_id=1, source_target_pairs={{0,1},{1,0},{2,3},{3,2},{4,5},{5,4},{6,7},{7,6}} | collective-permute-start | bytes 7077896 | tf_op jit(solution)/shard_map/ppermute | solution.py:35
  1355.9 39.6 %collective-permute-start.44 = (f32[2,384,768]{2,1,0:T(8,128)}, f32[2,384,768]{2,1,0:T(8,128)}, u32[]{:S(2)}, u32[]{:S(2)}) collective-permute-start(f32[2,384,768]{2,1,0:T(8,128)} %get-tuple-element.194), channel_id=1, source_target_pairs={{0,1},{1,0},{2,3},{3,2},{4,5},{5,4},{6,7},{7,6}} | collective-permute-start | bytes 7077896 | tf_op jit(solution)/shard_map/ppermute | solution.py:35
  1356.4 39.7 %collective-permute-start.45 = (f32[2,384,768]{2,1,0:T(8,128)}, f32[2,384,768]{2,1,0:T(8,128)}, u32[]{:S(2)}, u32[]{:S(2)}) collective-permute-start(f32[2,384,768]{2,1,0:T(8,128)} %get-tuple-element.195), channel_id=1, source_target_pairs={{0,1},{1,0},{2,3},{3,2},{4,5},{5,4},{6,7},{7,6}} | collective-permute-start | bytes 7077896 | tf_op jit(solution)/shard_map/ppermute | solution.py:35
  1363.8 85.2 %collective-permute-start.66 = (bf16[2048,1536]{1,0:T(8,128)(2,1)}, bf16[2048,1536]{1,0:T(8,128)(2,1)}, u32[]{:S(2)}, u32[]{:S(2)}) collective-permute-start(bf16[2048,1536]{1,0:T(8,128)(2,1)} %bitcast.28), channel_id=1, source_target_pairs={{0,1},{1,0},{2,3},{3,2},{4,5},{5,4},{6,7},{7,6}} | collective-permute-start | bytes 18874376 | tf_op jit(solution)/shard_map/ppermute | solution.py:35
  1392.5 210.6 %collective-permute-start.58 = (f32[2,384,768]{2,1,0:T(8,128)}, f32[2,384,768]{2,1,0:T(8,128)}, u32[]{:S(2)}, u32[]{:S(2)}) collective-permute-start(f32[2,384,768]{2,1,0:T(8,128)} %get-tuple-element.174), channel_id=1, source_target_pairs={{0,2},{2,0},{4,6},{6,4},{1,3},{3,1},{5,7},{7,5}} | collective-permute-start | bytes 7077896 | tf_op jit(solution)/shard_map/ppermute | solution.py:27
  1394.0 209.6 %collective-permute-start.60 = (f32[2,384,768]{2,1,0:T(8,128)}, f32[2,384,768]{2,1,0:T(8,128)}, u32[]{:S(2)}, u32[]{:S(2)}) collective-permute-start(f32[2,384,768]{2,1,0:T(8,128)} %add.354), channel_id=1, source_target_pairs={{0,4},{4,0},{2,6},{6,2},{1,5},{5,1},{3,7},{7,3}} | collective-permute-start | bytes 7077896 | tf_op jit(solution)/shard_map/ppermute | solution.py:31
  1395.5 179.0 %collective-permute-start.54 = (f32[2,384,768]{2,1,0:T(8,128)}, f32[2,384,768]{2,1,0:T(8,128)}, u32[]{:S(2)}, u32[]{:S(2)}) collective-permute-start(f32[2,384,768]{2,1,0:T(8,128)} %get-tuple-element.207), channel_id=1, source_target_pairs={{0,4},{4,0},{2,6},{6,2},{1,5},{5,1},{3,7},{7,3}} | collective-permute-start | bytes 7077896 | tf_op jit(solution)/shard_map/ppermute | solution.py:31
  1396.1 182.8 %collective-permute-start.51 = (f32[2,384,768]{2,1,0:T(8,128)}, f32[2,384,768]{2,1,0:T(8,128)}, u32[]{:S(2)}, u32[]{:S(2)}) collective-permute-start(f32[2,384,768]{2,1,0:T(8,128)} %get-tuple-element.203), channel_id=1, source_target_pairs={{0,2},{2,0},{4,6},{6,4},{1,3},{3,1},{5,7},{7,5}} | collective-permute-start | bytes 7077896 | tf_op jit(solution)/shard_map/ppermute | solution.py:27
  1419.0 155.6 %all-to-all-start.2 = ((bf16[8,512,768]{2,1,0:T(8,128)(2,1)}), bf16[8,512,768]{2,1,0:T(8,128)(2,1)}, u32[]{:S(2)}, u32[]{:S(2)}) async-start(bf16[8,512,768]{2,1,0:T(8,128)(2,1)} %get-tuple-element.218), calls=%async_computation.2 | async-start | bytes 12582912 | tf_op jit(solution)/shard_map/all_to_all | solution.py:611
  1449.0 176.0 %collective-permute-start.53 = (f32[2,384,768]{2,1,0:T(8,128)}, f32[2,384,768]{2,1,0:T(8,128)}, u32[]{:S(2)}, u32[]{:S(2)}) collective-permute-start(f32[2,384,768]{2,1,0:T(8,128)} %get-tuple-element.205), channel_id=1, source_target_pairs={{0,4},{4,0},{2,6},{6,2},{1,5},{5,1},{3,7},{7,3}} | collective-permute-start | bytes 7077896 | tf_op jit(solution)/shard_map/ppermute | solution.py:31
  1574.6 142.6 %collective-permute-start.65 = (f32[768,768]{1,0:T(8,128)S(1)}, f32[768,768]{1,0:T(8,128)}, u32[]{:S(2)}, u32[]{:S(2)}) collective-permute-start(f32[768,768]{1,0:T(8,128)S(1)} %bitcast.87), channel_id=1, source_target_pairs={{0,1},{1,0},{2,3},{3,2},{4,5},{5,4},{6,7},{7,6}} | collective-permute-start | bytes 7077896 | tf_op jit(solution)/shard_map/ppermute | solution.py:35
  1578.8 103.1 %collective-permute-start.69 = (bf16[1024,1536]{1,0:T(8,128)(2,1)}, bf16[1024,1536]{1,0:T(8,128)(2,1)}, u32[]{:S(2)}, u32[]{:S(2)}) collective-permute-start(bf16[1024,1536]{1,0:T(8,128)(2,1)} %constant_dynamic-update-slice_fusion), channel_id=1, source_target_pairs={{0,4},{2,6},{5,1},{7,3}} | collective-permute-start | bytes 9437192 | tf_op jit(solution)/shard_map/ppermute | solution.py:650
  1603.1 86.1 %collective-permute-start.50 = (f32[2,384,768]{2,1,0:T(8,128)}, f32[2,384,768]{2,1,0:T(8,128)}, u32[]{:S(2)}, u32[]{:S(2)}) collective-permute-start(f32[2,384,768]{2,1,0:T(8,128)} %get-tuple-element.201), channel_id=1, source_target_pairs={{0,2},{2,0},{4,6},{6,4},{1,3},{3,1},{5,7},{7,5}} | collective-permute-start | bytes 7077896 | tf_op jit(solution)/shard_map/ppermute | solution.py:27
  1603.7 104.5 %collective-permute-start.55 = (f32[2,384,768]{2,1,0:T(8,128)}, f32[2,384,768]{2,1,0:T(8,128)}, u32[]{:S(2)}, u32[]{:S(2)}) collective-permute-start(f32[2,384,768]{2,1,0:T(8,128)} %add.351), channel_id=1, source_target_pairs={{0,2},{2,0},{4,6},{6,4},{1,3},{3,1},{5,7},{7,5}} | collective-permute-start | bytes 7077896 | tf_op jit(solution)/shard_map/ppermute | solution.py:27
  1625.0 87.5 %collective-permute-start.52 = (f32[2,384,768]{2,1,0:T(8,128)}, f32[2,384,768]{2,1,0:T(8,128)}, u32[]{:S(2)}, u32[]{:S(2)}) collective-permute-start(f32[2,384,768]{2,1,0:T(8,128)} %add.348), channel_id=1, source_target_pairs={{0,4},{4,0},{2,6},{6,2},{1,5},{5,1},{3,7},{7,3}} | collective-permute-start | bytes 7077896 | tf_op jit(solution)/shard_map/ppermute | solution.py:31
  1682.0 103.7 %collective-permute-start.67 = (f32[768,1536]{1,0:T(8,128)}, f32[768,1536]{1,0:T(8,128)}, u32[]{:S(2)}, u32[]{:S(2)}) collective-permute-start(f32[768,1536]{1,0:T(8,128)} %add_add_fusion.refs_0_), channel_id=1, source_target_pairs={{0,1},{1,0},{2,3},{3,2},{4,5},{5,4},{6,7},{7,6}} | collective-permute-start | bytes 14155784 | tf_op jit(solution)/shard_map/ppermute | solution.py:35
  1689.2 82.9 %collective-permute-start.70 = (bf16[1024,1536]{1,0:T(8,128)(2,1)}, bf16[1024,1536]{1,0:T(8,128)(2,1)}, u32[]{:S(2)}, u32[]{:S(2)}) collective-permute-start(bf16[1024,1536]{1,0:T(8,128)(2,1)} %get-tuple-element.224), channel_id=1, source_target_pairs={{0,2},{2,0},{4,6},{6,4},{1,3},{3,1},{5,7},{7,5}} | collective-permute-start | bytes 9437192 | tf_op jit(solution)/shard_map/ppermute | solution.py:27
  1712.6 63.2 %collective-permute-start.57 = (f32[2,384,768]{2,1,0:T(8,128)}, f32[2,384,768]{2,1,0:T(8,128)}, u32[]{:S(2)}, u32[]{:S(2)}) collective-permute-start(f32[2,384,768]{2,1,0:T(8,128)} %add_add_fusion.3.own_b), channel_id=1, source_target_pairs={{0,1},{1,0},{2,3},{3,2},{4,5},{5,4},{6,7},{7,6}} | collective-permute-start | bytes 7077896 | tf_op jit(solution)/shard_map/ppermute | solution.py:35
  1717.2 58.6 %collective-permute-start.56 = (f32[2,384,768]{2,1,0:T(8,128)}, f32[2,384,768]{2,1,0:T(8,128)S(1)}, u32[]{:S(2)}, u32[]{:S(2)}) collective-permute-start(f32[2,384,768]{2,1,0:T(8,128)} %add_add_fusion.4.own_a), channel_id=1, source_target_pairs={{0,1},{1,0},{2,3},{3,2},{4,5},{5,4},{6,7},{7,6}} | collective-permute-start | bytes 7077896 | tf_op jit(solution)/shard_map/ppermute | solution.py:35
  (47 other events, 2662.3 us)
Sparse Core Ops, SparseCore 0:
  16.2 129.7 all-gather.5
  148.4 52.1 all-gather.7
  743.2 66.7 all-gather.9
  849.0 66.7 all-gather.11
  1042.2 135.9 all-gather.13

commit v8 on v7

--- a/solution.py
+++ b/solution.py
@@ -233,12 +233,17 @@
     )(x, e, wkv, *extra)
 
 
-def d_kv_body(acc0_ref, x_ref, e_ref, mid_ref, own_ref, recv_ref, w_ref, hist_ref, dkv_ref, prev_ref, acc_ref):
+def d_kv_body(layer, acc0_hbm, x_hbm, e_ref, um_hbm, own_ref, recv_ref, w_ref, hist_ref, dkv_ref, prev_ref,
+              acc_ref, acc0_ref, x_ref, mid_ref, sems):
     j = pl.program_id(0)
+    late = [pltpu.make_async_copy(src, dst, sems.at[n])
+            for n, (src, dst) in enumerate(((acc0_hbm, acc0_ref), (x_hbm, x_ref), (um_hbm.at[1, layer], mid_ref)))]
 
     @pl.when(j == 0)
     def _():
-        acc_ref[...] = acc0_ref[...]
+        for copy in late:
+            copy.start()
+        acc_ref[...] = jnp.zeros_like(acc_ref)
 
     dkv_ref[0, 0] = (own_ref[0] + recv_ref[0]).astype(BF16)
     for rows in ROWS:
@@ -246,27 +251,30 @@
 
     @pl.when(j == pl.num_programs(0) - 1)
     def _():
-        dn = acc_ref[...].astype(BF16).astype(F32)
+        for copy in late:
+            copy.wait()
+        dn = (acc_ref[...] + acc0_ref[...]).astype(BF16).astype(F32)
         s = x_ref[...].astype(F32) + e_ref[...]
         inv = lax.rsqrt(jnp.mean(s * s, axis=-1, keepdims=True) + EPS_NORM)
         proj = jnp.mean(s * dn, axis=-1, keepdims=True)
-        prev_ref[...] = (mid_ref[0, 0].astype(F32) + inv * dn - s * (inv * inv * inv * proj)).astype(BF16)
+        prev_ref[...] = (mid_ref[...].astype(F32) + inv * dn - s * (inv * inv * inv * proj)).astype(BF16)
 
 
 def d_kv(acc0, x, e, um_hist, own, recv, wkv, layer, layers, hist):
     t, dim = x.shape
     half = dim // 2
-    whole = pl.BlockSpec((t, dim), lambda j: (0, 0))
+    hbm = pl.BlockSpec(memory_space=pl.ANY)
     gblk = pl.BlockSpec((1, t, half), lambda j: (j // 2, 0, j % 2))
     return pl.pallas_call(
-        d_kv_body,
+        functools.partial(d_kv_body, layer),
         grid=(4,),
-        in_specs=[whole, whole, pl.BlockSpec((1, dim), lambda j: (0, 0)),
-                  pl.BlockSpec((1, 1, t, dim), lambda j: (1, layer, 0, 0)), gblk, gblk,
-                  pl.BlockSpec((half, dim), lambda j: (j, 0)), pl.BlockSpec(memory_space=pl.ANY)],
-        out_specs=[pl.BlockSpec((1, 1, t, half), lambda j: (1 + j // 2, layer, 0, j % 2)), whole],
+        in_specs=[hbm, hbm, pl.BlockSpec((1, dim), lambda j: (0, 0)), hbm, gblk, gblk,
+                  pl.BlockSpec((half, dim), lambda j: (j, 0)), hbm],
+        out_specs=[pl.BlockSpec((1, 1, t, half), lambda j: (1 + j // 2, layer, 0, j % 2)),
+                   pl.BlockSpec((t, dim), lambda j: (0, 0))],
         out_shape=[jax.ShapeDtypeStruct((4, layers, t, dim), BF16), jax.ShapeDtypeStruct((t, dim), BF16)],
-        scratch_shapes=[pltpu.VMEM((t, dim), F32)],
+        scratch_shapes=[pltpu.VMEM((t, dim), F32), pltpu.VMEM((t, dim), F32), pltpu.VMEM((t, dim), BF16),
+                        pltpu.VMEM((t, dim), BF16), pltpu.SemaphoreType.DMA((3,))],
         input_output_aliases={7: 0},
         compiler_params=pltpu.CompilerParams(dimension_semantics=('arbitrary',), vmem_limit_bytes=VMEM_ALL),
         cost_estimate=pl.CostEstimate(flops=4 * t * dim * dim, bytes_accessed=4 * dim * dim + 20 * t * dim, transcendentals=t),
@@ -274,63 +282,64 @@
     )(acc0, x, e, um_hist, own, recv, wkv, hist)
 
 
-def terms_body(added, places_ref, lhs_ref, rhs_ref, *refs):
+def terms_body(added, slot_of, places_ref, lhs_ref, rhs_ref, *refs):
     recv, outs = refs[:4 * added], refs[-4:]
-    step = 4 * pl.program_id(0) + pl.program_id(1)
+    step = pl.program_id(0)
     val = tn(lhs_ref[0], rhs_ref[0])
     for slot in range(4):
-        @pl.when(step // 2 == slot)
+        @pl.when(slot_of(step) == slot)
         def _():
             outs[slot][0] = val + recv[slot][0] if added else val
 
 
-def terms(lhs, rhs, rows, cols, places, lhs_at, rhs_at, chips, recv):
+def terms(lhs, rhs, rows, cols, places, plan, chips, recv):
     tokens = lhs.shape[1]
     first, second = chips
+    lhs_at, rhs_at, slot_of, turns = plan
 
     def rel(r):
         return first + r * (second - first)
 
-    slots = [pl.BlockSpec((1, rows, cols), lambda r, kind, p, at=2 * n: (jnp.clip(4 * r + kind - at, 0, 1), 0, 0))
-             for n in range(4)]
+    slots = [pl.BlockSpec((1, rows, cols), lambda i, p, at=at: (jnp.clip(i - at, 0, 1), 0, 0)) for at in turns]
     out = pl.pallas_call(
-        functools.partial(terms_body, len(recv) // 4),
+        functools.partial(terms_body, len(recv) // 4, slot_of),
         grid_spec=pltpu.PrefetchScalarGridSpec(
-            num_scalar_prefetch=1, grid=(2, 4),
-            in_specs=[pl.BlockSpec((1, tokens, rows), lambda r, kind, p: lhs_at(rel(r), kind, p)),
-                      pl.BlockSpec((1, tokens, cols), lambda r, kind, p: rhs_at(rel(r), kind, p))] + slots[:len(recv)],
+            num_scalar_prefetch=1, grid=(8,),
+            in_specs=[pl.BlockSpec((1, tokens, rows), lambda i, p: lhs_at(i, rel, p)),
+                      pl.BlockSpec((1, tokens, cols), lambda i, p: rhs_at(i, p))] + slots[:len(recv)],
             out_specs=slots),
         out_shape=[jax.ShapeDtypeStruct((2, rows, cols), F32)] * 4,
-        compiler_params=pltpu.CompilerParams(dimension_semantics=('arbitrary', 'arbitrary'), vmem_limit_bytes=VMEM_ALL),
+        compiler_params=pltpu.CompilerParams(dimension_semantics=('arbitrary',), vmem_limit_bytes=VMEM_ALL),
         cost_estimate=pl.CostEstimate(flops=16 * tokens * rows * cols, bytes_accessed=24 * tokens * rows, transcendentals=0),
     )(places, lhs, rhs, *recv)
     return {first: out[:2], second: out[2:]}
 
 
-def attn_lhs_at(rel, kind, p):
-    return kind, 0, rel
-
-
-def attn_rhs_at(rel, kind, p):
-    return kind // 3, 0, p[0]
-
-
-def up_lhs_at(rel, kind, p):
-    return 0, 0, 4 * p[1 + rel] + 2 * p[0] + kind % 2
-
-
-def up_rhs_at(rel, kind, p):
-    return 0, 0, kind // 2
-
-
-def summed_terms(lhs, rhs, rows, cols, places, lhs_at, rhs_at):
-    sent = {}
+ATTN_PLAN = (lambda i, rel, p: (jnp.where(i < 4, i % 2, i // 2), 0, rel(jnp.where(i < 4, i // 2, i % 2))),
+             lambda i, p: (i // 6, 0, p[0]),
+             lambda i: jnp.where(i < 4, 2 * (i // 2), 2 * (i % 2) + 1),
+             (0, 5, 2, 6))
+UP_PLAN = (lambda i, rel, p: (0, 0, 4 * p[1 + rel((i // 2) % 2)] + 2 * p[0] + i % 2),
+           lambda i, p: (0, 0, i // 4),
+           lambda i: 2 * ((i // 2) % 2) + i // 4,
+           (0, 4, 2, 6))
+
+
+def summed_terms(lhs, rhs, rows, cols, places, plan):
+    def in_turn(where, done):
+        return lax.optimization_barrier((where, done))[0] if done else where
+
+    sent, total = {}, {}
+    where, done = places[1], []
     for pair in ((3, 1), (2, 0)):
-        for r, ab in terms(lhs, rhs, rows, cols, places[1], lhs_at, rhs_at, pair, []).items():
-            sent[r] = [pp_d(v) for v in ab]
-    total = {}
+        out = terms(lhs, rhs, rows, cols, in_turn(where, done), plan, pair, [])
+        done = [v for ab in out.values() for v in ab]
+        sent.update({r: [pp_d(v) for v in ab] for r, ab in out.items()})
+    where, done = places[0], []
     for pair in ((3, 1), (2, 0)):
-        total.update(terms(lhs, rhs, rows, cols, places[0], lhs_at, rhs_at, pair, sent[pair[0]] + sent[pair[1]]))
+        out = terms(lhs, rhs, rows, cols, in_turn(where, done), plan, pair, sent[pair[0]] + sent[pair[1]])
+        done = [v for ab in out.values() for v in ab]
+        total.update(out)
     return total
 
 
@@ -403,12 +412,15 @@
 
 
 def mlp_bwd_body(*refs):
-    d_ref, h_ref, z_ref, wo_ref, w1_ref, w2_ref = refs[:6]
-    up_ref, mid_ref, dctx_ref, acc_ref = refs[-4:]
+    d_ref, h_hbm, z_ref, wo_hbm, w1_ref, w2_ref = refs[:6]
+    up_ref, mid_ref, dctx_ref, acc_ref, h_ref, wo_ref, sems = refs[-7:]
     j = pl.program_id(0)
+    late = [pltpu.make_async_copy(h_hbm, h_ref, sems.at[0]), pltpu.make_async_copy(wo_hbm, wo_ref, sems.at[1])]
 
     @pl.when(j == 0)
     def _():
+        for copy in late:
+            copy.start()
         acc_ref[...] = jnp.zeros_like(acc_ref)
 
     for i in range(0, BLOCK_B, SUB_B):
@@ -425,6 +437,8 @@
 
     @pl.when(j == pl.num_programs(0) - 1)
     def _():
+        for copy in late:
+            copy.wait()
         for rows in ROWS:
             dn = acc_ref[rows, :].astype(BF16).astype(F32)
             hf = h_ref[rows, :].astype(F32)
@@ -439,17 +453,19 @@
     t, dim = h.shape
     hidden = w2.shape[0]
     whole = pl.BlockSpec((t, dim), lambda j: (0, 0))
+    hbm = pl.BlockSpec(memory_space=pl.ANY)
     wblk = pl.BlockSpec((BLOCK_B, dim), lambda j: (j, 0))
     extra = [um_hist] if hist is None else [um_hist, hist]
     return pl.pallas_call(
         mlp_bwd_body,
         grid=(hidden // BLOCK_B,),
-        in_specs=[whole, whole, pl.BlockSpec((t, BLOCK_B), lambda j: (0, j)), pl.BlockSpec((dim, dim), lambda j: (0, 0)), wblk, wblk]
+        in_specs=[whole, hbm, pl.BlockSpec((t, BLOCK_B), lambda j: (0, j)), hbm, wblk, wblk]
         + [pl.BlockSpec(memory_space=pl.ANY)] * len(extra),
         out_specs=[pl.BlockSpec((1, t, BLOCK_B), lambda j: (layer, 0, j)), pl.BlockSpec((1, 1, t, dim), lambda j: (1, layer, 0, 0)), whole],
         out_shape=[jax.ShapeDtypeStruct((layers, t, hidden), BF16), jax.ShapeDtypeStruct((2, layers, t, dim), BF16),
                    jax.ShapeDtypeStruct((t, dim), BF16)],
-        scratch_shapes=[pltpu.VMEM((t, dim), F32)],
+        scratch_shapes=[pltpu.VMEM((t, dim), F32), pltpu.VMEM((t, dim), BF16), pltpu.VMEM((dim, dim), BF16),
+                        pltpu.SemaphoreType.DMA((2,))],
         input_output_aliases={6: 1} if hist is None else {6: 1, 7: 0},
         compiler_params=pltpu.CompilerParams(dimension_semantics=('arbitrary',), vmem_limit_bytes=VMEM_ALL),
         cost_estimate=pl.CostEstimate(flops=4 * t * dim * hidden, bytes_accessed=4 * dim * hidden + 4 * t * hidden,
@@ -479,11 +495,11 @@
 
 
 def join(core, own, other):
-    rows, cols = own.shape[0], own.shape[1] // 4
-    block = pl.BlockSpec((rows, cols), lambda i, j, c: (0, j))
+    rows, cols = own.shape[0] // 4, own.shape[1]
+    block = pl.BlockSpec((rows, cols), lambda i, j, c: (j, 0))
     return join_call(core, functools.partial(join_body, 1), (2, 4), [own], [other], [block],
-                     pl.BlockSpec((rows, cols), lambda i, j, c: ((c[0] + i) % 2, j)),
-                     jax.ShapeDtypeStruct((2 * rows, own.shape[1]), F32))
+                     pl.BlockSpec((rows, cols), lambda i, j, c: (4 * ((c[0] + i) % 2) + j, 0)),
+                     jax.ShapeDtypeStruct((8 * rows, cols), F32))
 
 
 def join_attn_body(core_ref, own_a, own_b, sib_a, sib_b, q_ref, k_ref, v_ref, o_ref):
@@ -556,6 +572,7 @@
         chips = (chip, nbr_x, nbr_y, diag)
         hid = w_q.shape[1]
         half_d = dim // 2
+        half_t = x_in.shape[1] // 2
 
         def take(v, which, axis, size):
             return lax.dynamic_slice_in_dim(v, which * size, size, axis)
@@ -626,7 +643,7 @@
                 next_all[layer] = gather(d_next)
             up_hist, um_hist, d_ctx = mlp_bwd(d_next, h, z, wo, w1, w2, layer, layer_count, um_hist, up_hist)
             if layer == 0:
-                total = summed_terms(flat(up_hist, 1), flat(m_hist, 1), hid, half_d, places, up_lhs_at, up_rhs_at)
+                total = summed_terms(flat(up_hist, 1), flat(m_hist, 1), hid, half_d, places, UP_PLAN)
                 d_ctx = after(d_ctx, *[v for r in (1, 2, 3) for v in total[r]])
                 own_1a = reduce_terms({r: v[0] for r, v in total.items()}, pp_x, pp_y, 1, 2)
                 own_1b = reduce_terms({r: v[1] for r, v in total.items()}, pp_y, pp_x, 2, 1)
@@ -635,23 +652,29 @@
             acc0 = nn(att_hist[0, layer], wq)
             att_hist, d_cur = d_kv(acc0, x_l, e, um_hist, own_kv, recv_kv, wkv, layer, layer_count, att_hist)
 
-        total = summed_terms(flat(att_hist, 4), flat(um_hist, 2), hid, half_d, places, attn_lhs_at, attn_rhs_at)
+        total = summed_terms(flat(att_hist, 4), flat(um_hist, 2), hid, half_d, places, ATTN_PLAN)
         own_qk = reduce_terms({r: v[0] for r, v in total.items()}, pp_x, pp_y, 1, 2)
         own_vo = reduce_terms({r: v[1] for r, v in total.items()}, pp_y, pp_x, 2, 1)
 
-        def ordered(own, sib, axis):
-            size = own.shape[axis]
-            shape = own.shape[:axis] + (2 * size,) + own.shape[axis + 1:]
-            return put(put(jnp.zeros(shape, own.dtype), own, core, axis), sib, 1 - core, axis)
+        at_home = chip_y == core
+        to_row = [(2 * c + d, 2 * (c ^ 2) + d) for c in range(4) for d in range(2) if c // 2 == d]
+        in_row = [(2 * c + d, 2 * (c ^ 1) + d) for c in range(4) for d in range(2) if c // 2 == d]
+
+        def in_order(mine, other):
+            return jnp.where(chip_x == 0, mine, other), jnp.where(chip_x == 0, other, mine)
 
         other_half = pp_d(d_cur)
-        whole = ordered(d_cur, other_half, 0)
-        to_row = [(2 * c + d, 2 * (c ^ 2) + d) for c in range(4) for d in range(2) if c // 2 == d]
-        from_y = lax.ppermute(whole, BOTH, to_row)
-        row_seq = jnp.where(chip_y == core, whole, from_y)
-        from_x = pp_x(row_seq)
-        d_x = jnp.zeros((2,) + whole.shape, BF16)
-        d_x = put(put(d_x, row_seq[None], chip_x, 0), from_x[None], 1 - chip_x, 0)
+        part_p = jnp.where(core == 0, d_cur, other_half)
+        part_q = jnp.where(core == 0, other_half, d_cur)
+        p_y = lax.ppermute(part_p, BOTH, to_row)
+        q_x = lax.ppermute(part_q, BOTH, in_row)
+        p_row = jnp.where(at_home, part_p, p_y)
+        q_row = jnp.concatenate(in_order(part_q, q_x), axis=0)
+        p_x = pp_x(p_row)
+        q_y = lax.ppermute(q_row, BOTH, to_row)
+        q_both = jnp.where(at_home, q_row, q_y)
+        p_0, p_1 = in_order(p_row, p_x)
+        d_x = jnp.concatenate([p_0, q_both[:half_t], p_1, q_both[half_t:]], axis=0).reshape(2, -1, dim)
 
         ready = tuple(v for ab in total.values() for v in ab)
         cot_mine = cot_out.reshape(-1, dim)

time: 1810 us -> 1750 us (0.967)
  waiting for transfers between devices: 588 us -> 537 us
  Pallas kernels: 852 us -> 825 us
    all_to_all x4, waiting for transfers between devices: 123 us -> 6.76 us  [device_step(): lax.all_to_all(g.reshape(-1, g.shape[-1]), BOTH, split_axis=0, concat_axi...]
    ppermute x13, waiting for transfers between devices: 195 us -> 286 us  [pp_x(): return lax.ppermute(v, 'model', SWAP_X)]
    ppermute x1 -> x3, waiting for transfers between devices: 34.8 us -> 0.01 us  [the longest x1 0.01 us: device_step(): q_x = lax.ppermute(part_q, BOTH, in_row)]
    ppermute x1 -> x3, starting transfers between devices: 4.16 us -> 29.9 us  [the longest x1 20.2 us: device_step(): q_x = lax.ppermute(part_q, BOTH, in_row)]
    dynamic_update_slice x29 -> x26, local copies, waits for them, and re-layouts: 50.7 us -> 42.9 us  [put(): return lax.dynamic_update_slice_in_dim(buf, v, which * v.shape[axis], axis)]
  transfers between devices with their start and end apart: 80 -> 82, of which waited for: 24 -> 23; matrix products, arithmetic and copies ran while one was open for 15% -> 16% of each run, Pallas kernels for 27% -> 27%
where the time goes in v8:
time: 1750 us; the launch traced here: 1740 us
  Pallas kernels  825 us (47%)
  waiting for transfers between devices  537 us (31%)
  matrix products  124 us (7%)
  local copies, waits for them, and re-layouts  108 us (6%)
  starting transfers between devices  77.6 us (4%)
  other arithmetic  52.7 us (3%)
    ppermute x13, waiting for transfers between devices, pp_x(): return lax.ppermute(v, 'model', SWAP_X)  286 us
    ppermute x12, waiting for transfers between devices, pp_y(): return lax.ppermute(v, 'model', SWAP_Y)  228 us
    pallas_call x4, Pallas kernels, attn_bwd(): pl.pallas_call(attn_bwd_body, grid=(steps,), in_specs=[qblk, kblk, kblk,...  168 us
    pallas_call x8, Pallas kernels, terms(): pl.pallas_call(functools.partial(terms_body, len(recv) // 4, slot_of), gr...  163 us
    pallas_call x4, Pallas kernels, mlp_bwd(): pl.pallas_call(mlp_bwd_body, grid=(hidden // BLOCK_B,), in_specs=[whole,...  138 us
    pallas_call x4, Pallas kernels, mlp_fwd(): pl.pallas_call(mlp_fwd_body, grid=(hidden // BLOCK_F,), in_specs=[whole,...  134 us
    dot_general x13, matrix products, dot(): return lax.dot_general(a, b, (dims, ((), ())), preferred_element_type=F32)  124 us
    pallas_call x4, Pallas kernels, attn_fwd(): pl.pallas_call(attn_fwd_body, grid=(pairs,), in_specs=[pl.BlockSpec((tq,...  94.5 us
  transfers between devices with their start and end apart: 82, of which 23 were waited for; matrix products, arithmetic and copies ran while one was open for 16% of the time, Pallas kernels for 27%

profile of v8, /device:TPU:0, one launch (start us, length us, event | category | flops | bytes accessed | tf_op | source)
XLA Modules:
  0.0 1738.8 jit_solution(5879749871544520605)
XLA Ops:
  16.2 6.6 copy.43
  39.8 7.3 broadcast.6.clone
  50.2 26.4 %collective-permute-done.2 = bf16[384,1536]{1,0:T(8,128)(2,1)} collective-permute-done((bf16[384,1536]{1,0:T(8,128)(2,1)}, bf16[384,1536]{1,0:T(8,128)(2,1)}, u32[]{:S(2)}, u32[]{:S(2)}) %collective-permute-start.2) | collective-permute-done | bytes 1179680 | tf_op jit(solution)/shard_map/ppermute | solution.py:27
  77.1 6.5 broadcast.6.clone.1
  86.1 41.1 %collective-permute-done.4 = bf16[384,1536]{1,0:T(8,128)(2,1)} collective-permute-done((bf16[384,1536]{1,0:T(8,128)(2,1)}, bf16[384,1536]{1,0:T(8,128)(2,1)}, u32[]{:S(2)}, u32[]{:S(2)}) %collective-permute-start.4) | collective-permute-done | bytes 1179680 | tf_op jit(solution)/shard_map/ppermute | solution.py:27
  131.8 34.3 %collective-permute-done.14 = bf16[384,1536]{1,0:T(8,128)(2,1)} collective-permute-done((bf16[384,1536]{1,0:T(8,128)(2,1)}, bf16[384,1536]{1,0:T(8,128)(2,1)}, u32[]{:S(2)}, u32[]{:S(2)}) %collective-permute-start.14) | collective-permute-done | bytes 1179680 | tf_op jit(solution)/shard_map/ppermute | solution.py:27
  175.3 29.9 %collective-permute-done.16 = bf16[384,1536]{1,0:T(8,128)(2,1)S(1)} collective-permute-done((bf16[384,1536]{1,0:T(8,128)(2,1)S(1)}, bf16[384,1536]{1,0:T(8,128)(2,1)S(1)}, u32[]{:S(2)}, u32[]{:S(2)}) %collective-permute-start.16) | collective-permute-done | bytes 1179680 | tf_op jit(solution)/shard_map/ppermute | solution.py:27
  217.1 19.4 %collective-permute-done.20 = bf16[384,1536]{1,0:T(8,128)(2,1)S(1)} collective-permute-done((bf16[384,1536]{1,0:T(8,128)(2,1)S(1)}, bf16[384,1536]{1,0:T(8,128)(2,1)S(1)}, u32[]{:S(2)}, u32[]{:S(2)}) %collective-permute-start.20) | collective-permute-done | bytes 1179680 | tf_op jit(solution)/shard_map/ppermute | solution.py:31
  244.5 17.3 collective-permute-done.10
  265.4 21.2 %collective-permute-done.22 = bf16[384,1536]{1,0:T(8,128)(2,1)} collective-permute-done((bf16[384,1536]{1,0:T(8,128)(2,1)}, bf16[384,1536]{1,0:T(8,128)(2,1)}, u32[]{:S(2)}, u32[]{:S(2)}) %collective-permute-start.22) | collective-permute-done | bytes 1179680 | tf_op jit(solution)/shard_map/ppermute | solution.py:31
  313.5 10.8 norm_kv.4
  340.9 7.7 convolution_convert_fusion.3.refs_0_.refs_1_.q_ref
  348.6 23.6 %attn_fwd.4 = (bf16[4,4,512,1536]{3,2,1,0:T(8,128)(2,1)}, f32[12,2,512]{2,1,0:T(2,128)}) custom-call(bf16[512,1536]{1,0:T(8,128)(2,1)} %convolution_convert_fusion.3.refs_0_.refs_1_.q_ref, bf16[512,1536]{1,0:T(8,128)(2,1)} %convolution_convert_fusion.3.refs_0_.refs_1_.q_ref, bf16[512,3072]{1,0:T(8,128)(2,1)} %get-tuple-element.120.refs_2_.refs_4_.refs_6_.ko_ref.vo_ref, ...), custom_call_target="tpu_custom_call" | custom-call | flops 12884901888 | bytes 9437184 | tf_op jit(solution)/shard_map/attn_fwd/pallas_call | solution.py:114
  372.2 33.6 %mlp_fwd.4 = (bf16[512,6144]{1,0:T(8,128)(2,1)}, bf16[8,512,768]{2,1,0:T(8,128)(2,1)}, bf16[512,1536]{1,0:T(8,128)(2,1)}, bf16[512,1536]{1,0:T(8,128)(2,1)}, bf16[4,512,1536]{2,1,0:T(8,128)(2,1)}) custom-call(bf16[512,1536]{1,0:T(8,128)(2,1)} %bitcast_select_fusion.1.refs_0_.x_hbm, f32[1,1536]{1,0:T(1,128)} %get-tuple-element.255.refs_1_.e_ref, ...), custom_call_target="tpu_custom_call" | custom-call | flops 19327352832 | bytes 50331648 | tf_op jit(solution)/shard_map/mlp_fwd/pallas_call | solution.py:389
  405.8 10.1 norm_kv.5
  421.8 23.6 %attn_fwd.5 = (bf16[4,4,512,1536]{3,2,1,0:T(8,128)(2,1)}, f32[12,2,512]{2,1,0:T(2,128)}) custom-call(bf16[512,1536]{1,0:T(8,128)(2,1)} %convolution_convert_fusion.2.refs_0_.refs_1_.q_ref, bf16[512,1536]{1,0:T(8,128)(2,1)} %convolution_convert_fusion.2.refs_0_.refs_1_.q_ref, ...), custom_call_target="tpu_custom_call", output_to_operand_aliasing={{0}: (8, {})} | custom-call | flops 12884901888 | bytes 9437184 | tf_op jit(solution)/shard_map/attn_fwd/pallas_call | solution.py:114
  445.4 33.6 %mlp_fwd.5 = (bf16[512,6144]{1,0:T(8,128)(2,1)}, bf16[8,512,768]{2,1,0:T(8,128)(2,1)}, bf16[512,1536]{1,0:T(8,128)(2,1)}, bf16[512,1536]{1,0:T(8,128)(2,1)}, bf16[4,512,1536]{2,1,0:T(8,128)(2,1)}) custom-call(bf16[512,1536]{1,0:T(8,128)(2,1)} %get-tuple-element.122.refs_0_.x_hbm, ...), custom_call_target="tpu_custom_call", output_to_operand_aliasing={{4}: (6, {})} | custom-call | flops 19327352832 | bytes 50331648 | tf_op jit(solution)/shard_map/mlp_fwd/pallas_call | solution.py:389
  479.0 9.9 norm_kv.6
  494.9 23.8 %attn_fwd.6 = (bf16[4,4,512,1536]{3,2,1,0:T(8,128)(2,1)}, f32[12,2,512]{2,1,0:T(2,128)}) custom-call(bf16[512,1536]{1,0:T(8,128)(2,1)} %convolution_convert_fusion.1.refs_0_.refs_1_.q_ref, bf16[512,1536]{1,0:T(8,128)(2,1)} %convolution_convert_fusion.1.refs_0_.refs_1_.q_ref, ...), custom_call_target="tpu_custom_call", output_to_operand_aliasing={{0}: (8, {})} | custom-call | flops 12884901888 | bytes 9437184 | tf_op jit(solution)/shard_map/attn_fwd/pallas_call | solution.py:114
  518.7 33.6 %mlp_fwd.6 = (bf16[512,6144]{1,0:T(8,128)(2,1)}, bf16[8,512,768]{2,1,0:T(8,128)(2,1)}, bf16[512,1536]{1,0:T(8,128)(2,1)}, bf16[512,1536]{1,0:T(8,128)(2,1)}, bf16[4,512,1536]{2,1,0:T(8,128)(2,1)}) custom-call(bf16[512,1536]{1,0:T(8,128)(2,1)} %get-tuple-element.127.refs_0_.x_hbm, ...), custom_call_target="tpu_custom_call", output_to_operand_aliasing={{4}: (6, {})} | custom-call | flops 19327352832 | bytes 50331648 | tf_op jit(solution)/shard_map/mlp_fwd/pallas_call | solution.py:389
  552.3 10.0 norm_kv.7
  564.6 5.8 collective-permute-done.29
  573.5 7.7 convolution_convert_fusion.refs_0_.refs_1_.q_ref
  581.2 23.6 %attn_fwd.7 = (bf16[4,4,512,1536]{3,2,1,0:T(8,128)(2,1)}, f32[12,2,512]{2,1,0:T(2,128)}) custom-call(bf16[512,1536]{1,0:T(8,128)(2,1)} %convolution_convert_fusion.refs_0_.refs_1_.q_ref, bf16[512,1536]{1,0:T(8,128)(2,1)} %convolution_convert_fusion.refs_0_.refs_1_.q_ref, ...), custom_call_target="tpu_custom_call", output_to_operand_aliasing={{0}: (8, {})} | custom-call | flops 12884901888 | bytes 9437184 | tf_op jit(solution)/shard_map/attn_fwd/pallas_call | solution.py:114
  604.8 33.5 %mlp_fwd.7 = (bf16[512,6144]{1,0:T(8,128)(2,1)}, bf16[8,512,768]{2,1,0:T(8,128)(2,1)}, bf16[512,1536]{1,0:T(8,128)(2,1)}, bf16[512,1536]{1,0:T(8,128)(2,1)}, bf16[4,512,1536]{2,1,0:T(8,128)(2,1)}) custom-call(bf16[512,1536]{1,0:T(8,128)(2,1)} %get-tuple-element.132.refs_0_.x_hbm, ...), custom_call_target="tpu_custom_call", output_to_operand_aliasing={{4}: (6, {})} | custom-call | flops 19327352832 | bytes 50331648 | tf_op jit(solution)/shard_map/mlp_fwd/pallas_call | solution.py:389
  638.3 34.0 %mlp_bwd.4 = (bf16[4,512,6144]{2,1,0:T(8,128)(2,1)}, bf16[2,4,512,1536]{3,2,1,0:T(8,128)(2,1)}, bf16[512,1536]{1,0:T(8,128)(2,1)}) custom-call(bf16[512,1536]{1,0:T(8,128)(2,1)} %bitcast_select_fusion.refs_0_, bf16[512,1536]{1,0:T(8,128)(2,1)} %get-tuple-element.137.refs_1_, ...), custom_call_target="tpu_custom_call", output_to_operand_aliasing={{1}: (6, {})} | custom-call | flops 19327352832 | bytes 50331648 | tf_op jit(solution)/shard_map/mlp_bwd/pallas_call | solution.py:459
  672.3 42.3 %attn_bwd.4 = (bf16[4,4,512,1536]{3,2,1,0:T(8,128)(2,1)}, f32[2,512,1536]{2,1,0:T(8,128)}, f32[2,512,1536]{2,1,0:T(8,128)}) custom-call(bf16[512,1536]{1,0:T(8,128)(2,1)} %convolution_convert_fusion.refs_0_.refs_1_.q_ref, bf16[512,3072]{1,0:T(8,128)(2,1)} %get-tuple-element.134.refs_2_.refs_4_.refs_6_.ko_ref.vo_ref, ...), custom_call_target="tpu_custom_call", output_to_operand_aliasing={{0}: (7, {})} | custom-call | flops 32212254720 | bytes 25165824 | tf_op jit(solution)/shard_map/attn_bwd/pallas_call | solution.py:186
  714.7 6.0 fusion.13.acc0_hbm
  725.1 14.5 d_kv.4
  739.6 34.5 %mlp_bwd.5 = (bf16[4,512,6144]{2,1,0:T(8,128)(2,1)}, bf16[2,4,512,1536]{3,2,1,0:T(8,128)(2,1)}, bf16[512,1536]{1,0:T(8,128)(2,1)}) custom-call(bf16[512,1536]{1,0:T(8,128)(2,1)} %get-tuple-element.145.refs_0_, bf16[512,1536]{1,0:T(8,128)(2,1)} %get-tuple-element.146.refs_1_, ...), custom_call_target="tpu_custom_call", output_to_operand_aliasing={{1}: (6, {}), {0}: (7, {})} | custom-call | flops 19327352832 | bytes 50331648 | tf_op jit(solution)/shard_map/mlp_bwd/pallas_call | solution.py:459
  774.2 41.9 %attn_bwd.5 = (bf16[4,4,512,1536]{3,2,1,0:T(8,128)(2,1)}, f32[2,512,1536]{2,1,0:T(8,128)}, f32[2,512,1536]{2,1,0:T(8,128)}) custom-call(bf16[512,1536]{1,0:T(8,128)(2,1)} %convolution_convert_fusion.1.refs_0_.refs_1_.q_ref, bf16[512,3072]{1,0:T(8,128)(2,1)} %get-tuple-element.129.refs_2_.refs_4_.refs_6_.ko_ref.vo_ref, ...), custom_call_target="tpu_custom_call", output_to_operand_aliasing={{0}: (7, {})} | custom-call | flops 32212254720 | bytes 25165824 | tf_op jit(solution)/shard_map/attn_bwd/pallas_call | solution.py:186
  816.1 6.0 fusion.11.acc0_hbm
  826.6 14.5 d_kv.5
  841.1 34.9 %mlp_bwd.6 = (bf16[4,512,6144]{2,1,0:T(8,128)(2,1)}, bf16[2,4,512,1536]{3,2,1,0:T(8,128)(2,1)}, bf16[512,1536]{1,0:T(8,128)(2,1)}) custom-call(bf16[512,1536]{1,0:T(8,128)(2,1)} %get-tuple-element.156.refs_0_, bf16[512,1536]{1,0:T(8,128)(2,1)} %get-tuple-element.157.refs_1_, ...), custom_call_target="tpu_custom_call", output_to_operand_aliasing={{1}: (6, {}), {0}: (7, {})} | custom-call | flops 19327352832 | bytes 50331648 | tf_op jit(solution)/shard_map/mlp_bwd/pallas_call | solution.py:459
  876.0 41.9 %attn_bwd.6 = (bf16[4,4,512,1536]{3,2,1,0:T(8,128)(2,1)}, f32[2,512,1536]{2,1,0:T(8,128)}, f32[2,512,1536]{2,1,0:T(8,128)}) custom-call(bf16[512,1536]{1,0:T(8,128)(2,1)} %convolution_convert_fusion.2.refs_0_.refs_1_.q_ref, bf16[512,3072]{1,0:T(8,128)(2,1)} %get-tuple-element.124.refs_2_.refs_4_.refs_6_.ko_ref.vo_ref, ...), custom_call_target="tpu_custom_call", output_to_operand_aliasing={{0}: (7, {})} | custom-call | flops 32212254720 | bytes 25165824 | tf_op jit(solution)/shard_map/attn_bwd/pallas_call | solution.py:186
  922.4 6.0 fusion.9.acc0_hbm
  928.5 14.6 d_kv.6
  943.1 34.1 %mlp_bwd.7 = (bf16[4,512,6144]{2,1,0:T(8,128)(2,1)}, bf16[2,4,512,1536]{3,2,1,0:T(8,128)(2,1)}, bf16[512,1536]{1,0:T(8,128)(2,1)}) custom-call(bf16[512,1536]{1,0:T(8,128)(2,1)} %get-tuple-element.167.refs_0_, bf16[512,1536]{1,0:T(8,128)(2,1)} %get-tuple-element.168.refs_1_, ...), custom_call_target="tpu_custom_call", output_to_operand_aliasing={{1}: (6, {}), {0}: (7, {})} | custom-call | flops 19327352832 | bytes 50331648 | tf_op jit(solution)/shard_map/mlp_bwd/pallas_call | solution.py:459
  977.2 19.5 %shard_map.144 = (f32[2,384,768]{2,1,0:T(8,128)}, f32[2,384,768]{2,1,0:T(8,128)}, f32[2,384,768]{2,1,0:T(8,128)}, f32[2,384,768]{2,1,0:T(8,128)}) custom-call(s32[5]{0:T(128)} %stack.32.places_ref, bf16[1,2048,6144]{2,1,0:T(8,128)(2,1)} %bitcast.72, bf16[1,2048,1536]{2,1,0:T(8,128)(2,1)} %bitcast.76), custom_call_target="tpu_custom_call" | custom-call | flops 9663676416 | bytes 18874368 | tf_op jit(solution)/shard_map/pallas_call | solution.py:304
  997.7 19.7 %shard_map.146 = (f32[2,384,768]{2,1,0:T(8,128)}, f32[2,384,768]{2,1,0:T(8,128)}, f32[2,384,768]{2,1,0:T(8,128)}, f32[2,384,768]{2,1,0:T(8,128)}) custom-call(s32[5]{0:T(128)} %stack.32.places_ref, bf16[1,2048,6144]{2,1,0:T(8,128)(2,1)} %bitcast.73, bf16[1,2048,1536]{2,1,0:T(8,128)(2,1)} %bitcast.77), custom_call_target="tpu_custom_call" | custom-call | flops 9663676416 | bytes 18874368 | tf_op jit(solution)/shard_map/pallas_call | solution.py:304
  1019.0 21.1 %shard_map.145 = (f32[2,384,768]{2,1,0:T(8,128)}, f32[2,384,768]{2,1,0:T(8,128)}, f32[2,384,768]{2,1,0:T(8,128)}, f32[2,384,768]{2,1,0:T(8,128)}) custom-call(s32[5]{0:T(128)} %stack.30.places_ref, bf16[1,2048,6144]{2,1,0:T(8,128)(2,1)} %bitcast.74, bf16[1,2048,1536]{2,1,0:T(8,128)(2,1)} %bitcast.78, f32[2,384,768]{2,1,0:T(8,128)} %collective-permute-done.33.refs_0_, ...), custom_call_target="tpu_custom_call" | custom-call | flops 9663676416 | bytes 18874368 | tf_op jit(solution)/shard_map/pallas_call | solution.py:304
  1045.0 21.1 %shard_map.147 = (f32[2,384,768]{2,1,0:T(8,128)}, f32[2,384,768]{2,1,0:T(8,128)}, f32[2,384,768]{2,1,0:T(8,128)}, f32[2,384,768]{2,1,0:T(8,128)}) custom-call(s32[5]{0:T(128)} %stack.30.places_ref, bf16[1,2048,6144]{2,1,0:T(8,128)(2,1)} %bitcast.75, bf16[1,2048,1536]{2,1,0:T(8,128)(2,1)} %bitcast.79, f32[2,384,768]{2,1,0:T(8,128)} %copy-done.17, ...), custom_call_target="tpu_custom_call" | custom-call | flops 9663676416 | bytes 18874368 | tf_op jit(solution)/shard_map/pallas_call | solution.py:304
  1066.2 41.8 %attn_bwd.7 = (bf16[4,4,512,1536]{3,2,1,0:T(8,128)(2,1)}, f32[2,512,1536]{2,1,0:T(8,128)}, f32[2,512,1536]{2,1,0:T(8,128)}) custom-call(bf16[512,1536]{1,0:T(8,128)(2,1)} %convolution_convert_fusion.3.refs_0_.refs_1_.q_ref, bf16[512,3072]{1,0:T(8,128)(2,1)} %get-tuple-element.120.refs_2_.refs_4_.refs_6_.ko_ref.vo_ref, ...), custom_call_target="tpu_custom_call", output_to_operand_aliasing={{0}: (7, {})} | custom-call | flops 32212254720 | bytes 25165824 | tf_op jit(solution)/shard_map/attn_bwd/pallas_call | solution.py:186
  1108.4 6.7 all-to-all-done.1
  1123.5 163.6 %collective-permute-done.62 = f32[2,384,768]{2,1,0:T(8,128)S(1)} collective-permute-done((f32[2,384,768]{2,1,0:T(8,128)}, f32[2,384,768]{2,1,0:T(8,128)S(1)}, u32[]{:S(2)}, u32[]{:S(2)}) %collective-permute-start.62) | collective-permute-done | bytes 2359328 | tf_op jit(solution)/shard_map/ppermute | solution.py:31
  1297.9 14.7 d_kv.7
  1312.6 19.2 %shard_map.148 = (f32[2,384,768]{2,1,0:T(8,128)}, f32[2,384,768]{2,1,0:T(8,128)}, f32[2,384,768]{2,1,0:T(8,128)}, f32[2,384,768]{2,1,0:T(8,128)}) custom-call(s32[5]{0:T(128)} %stack.32.places_ref, bf16[4,2048,1536]{2,1,0:T(8,128)(2,1)} %bitcast.64, bf16[2,2048,1536]{2,1,0:T(8,128)(2,1)} %bitcast.68), custom_call_target="tpu_custom_call" | custom-call | flops 9663676416 | bytes 18874368 | tf_op jit(solution)/shard_map/pallas_call | solution.py:304
  1331.9 5.9 collective-permute-done.61
  1341.8 46.0 %collective-permute-done.63 = f32[2,384,768]{2,1,0:T(8,128)} collective-permute-done((f32[2,384,768]{2,1,0:T(8,128)}, f32[2,384,768]{2,1,0:T(8,128)}, u32[]{:S(2)}, u32[]{:S(2)}) %collective-permute-start.63) | collective-permute-done | bytes 2359328 | tf_op jit(solution)/shard_map/ppermute | solution.py:27
  1388.4 19.3 %shard_map.150 = (f32[2,384,768]{2,1,0:T(8,128)}, f32[2,384,768]{2,1,0:T(8,128)}, f32[2,384,768]{2,1,0:T(8,128)}, f32[2,384,768]{2,1,0:T(8,128)}) custom-call(s32[5]{0:T(128)} %stack.32.places_ref, bf16[4,2048,1536]{2,1,0:T(8,128)(2,1)} %bitcast.65, bf16[2,2048,1536]{2,1,0:T(8,128)(2,1)} %bitcast.69), custom_call_target="tpu_custom_call" | custom-call | flops 9663676416 | bytes 18874368 | tf_op jit(solution)/shard_map/pallas_call | solution.py:304
  1421.3 21.3 %shard_map.149 = (f32[2,384,768]{2,1,0:T(8,128)}, f32[2,384,768]{2,1,0:T(8,128)}, f32[2,384,768]{2,1,0:T(8,128)}, f32[2,384,768]{2,1,0:T(8,128)}) custom-call(s32[5]{0:T(128)} %stack.30.places_ref, bf16[4,2048,1536]{2,1,0:T(8,128)(2,1)} %bitcast.66, bf16[2,2048,1536]{2,1,0:T(8,128)(2,1)} %bitcast.70, f32[2,384,768]{2,1,0:T(8,128)} %copy-done.9, ...), custom_call_target="tpu_custom_call" | custom-call | flops 9663676416 | bytes 18874368 | tf_op jit(solution)/shard_map/pallas_call | solution.py:304
  1443.1 20.2 %collective-permute-start.71 = (bf16[512,1536]{1,0:T(8,128)(2,1)S(1)}, bf16[512,1536]{1,0:T(8,128)(2,1)}, u32[]{:S(2)}, u32[]{:S(2)}) collective-permute-start(bf16[512,1536]{1,0:T(8,128)(2,1)S(1)} %get-tuple-element.247), channel_id=1, source_target_pairs={{0,2},{2,0},{5,7},{7,5}} | collective-permute-start | bytes 4718600 | tf_op jit(solution)/shard_map/ppermute | solution.py:670
  1463.3 21.5 %shard_map.151 = (f32[2,384,768]{2,1,0:T(8,128)}, f32[2,384,768]{2,1,0:T(8,128)}, f32[2,384,768]{2,1,0:T(8,128)}, f32[2,384,768]{2,1,0:T(8,128)}) custom-call(s32[5]{0:T(128)} %stack.30.places_ref, bf16[4,2048,1536]{2,1,0:T(8,128)(2,1)} %bitcast.67, bf16[2,2048,1536]{2,1,0:T(8,128)(2,1)} %bitcast.71, f32[2,384,768]{2,1,0:T(8,128)} %collective-permute-done.46.refs_0_, ...), custom_call_target="tpu_custom_call" | custom-call | flops 9663676416 | bytes 18874368 | tf_op jit(solution)/shard_map/pallas_call | solution.py:304
  1484.9 10.0 fusion.2
  1494.8 16.4 fusion.32
  1511.7 10.0 fusion
  1534.9 30.1 %collective-permute-done.51 = f32[2,384,768]{2,1,0:T(8,128)S(1)} collective-permute-done((f32[2,384,768]{2,1,0:T(8,128)S(1)}, f32[2,384,768]{2,1,0:T(8,128)S(1)}, u32[]{:S(2)}, u32[]{:S(2)}) %collective-permute-start.51) | collective-permute-done | bytes 2359328 | tf_op jit(solution)/shard_map/ppermute | solution.py:27
  1567.2 16.5 fusion.33
  1589.4 21.6 %add_add_fusion.refs_0_ = f32[768,1536]{1,0:T(8,128)} fusion(f32[768,1536]{1,0:T(8,128)} %fusion.33, f32[768,1536]{1,0:T(8,128)} %fusion.32, f32[768,1536]{1,0:T(8,128)} %fusion.2, f32[768,1536]{1,0:T(8,128)} %fusion, bf16[4096,768]{1,0:T(8,128)(2,1)} %bitcast.31, bf16[4096,1536]{1,0:T(8,128)(2,1)} %all-gather.14.cloned.1.call-done), kind=kOutput, calls=%fused_computation.4 | convolution fusion | flops 9668395008 | bytes 42467328 | tf_op jit(solution)/shard_map/dot_general | solution.py:39
  1614.1 54.7 %collective-permute-done.55 = f32[2,384,768]{2,1,0:T(8,128)} collective-permute-done((f32[2,384,768]{2,1,0:T(8,128)}, f32[2,384,768]{2,1,0:T(8,128)}, u32[]{:S(2)}, u32[]{:S(2)}) %collective-permute-start.55) | collective-permute-done | bytes 2359328 | tf_op jit(solution)/shard_map/ppermute | solution.py:27
  1669.1 8.7 shard_map.153
  1685.3 19.1 %collective-permute-done.70 = bf16[512,1536]{1,0:T(8,128)(2,1)} collective-permute-done((bf16[512,1536]{1,0:T(8,128)(2,1)}, bf16[512,1536]{1,0:T(8,128)(2,1)}, u32[]{:S(2)}, u32[]{:S(2)}) %collective-permute-start.70) | collective-permute-done | bytes 1572896 | tf_op jit(solution)/shard_map/ppermute | solution.py:27
  1712.0 8.5 shard_map.152
  1720.5 11.6 shard_map.154
  (297 shorter events, 229.3 us)
Async XLA Ops:
  7.2 288.3 %all-gather.6.cloned.1.call-start = ((), (), s32[]{:S(2)}) async-start(), calls=%async_computation.4 | async-start | bytes 15925248 | tf_op jit(solution)/shard_map/all_gather | solution.py:584
  16.1 319.3 %all-gather.8.cloned.1.call-start = ((), (), s32[]{:S(2)}) async-start(), calls=%async_computation.5 | async-start | bytes 5308416 | tf_op jit(solution)/shard_map/all_gather | solution.py:584
  26.5 50.1 %collective-permute-start.2 = (bf16[384,1536]{1,0:T(8,128)(2,1)}, bf16[384,1536]{1,0:T(8,128)(2,1)}, u32[]{:S(2)}, u32[]{:S(2)}) collective-permute-start(bf16[384,1536]{1,0:T(8,128)(2,1)} %get-tuple-element.251), channel_id=1, source_target_pairs={{0,2},{2,0},{4,6},{6,4},{1,3},{3,1},{5,7},{7,5}} | collective-permute-start | bytes 3538952 | tf_op jit(solution)/shard_map/ppermute | solution.py:27
  29.9 100.3 %collective-permute-start.6 = (bf16[384,1536]{1,0:T(8,128)(2,1)}, bf16[384,1536]{1,0:T(8,128)(2,1)}, u32[]{:S(2)}, u32[]{:S(2)}) collective-permute-start(bf16[384,1536]{1,0:T(8,128)(2,1)} %get-tuple-element.251), channel_id=1, source_target_pairs={{0,4},{4,0},{2,6},{6,2},{1,5},{5,1},{3,7},{7,3}} | collective-permute-start | bytes 3538952 | tf_op jit(solution)/shard_map/ppermute | solution.py:31
  31.4 95.8 %collective-permute-start.4 = (bf16[384,1536]{1,0:T(8,128)(2,1)}, bf16[384,1536]{1,0:T(8,128)(2,1)}, u32[]{:S(2)}, u32[]{:S(2)}) collective-permute-start(bf16[384,1536]{1,0:T(8,128)(2,1)} %get-tuple-element.250), channel_id=1, source_target_pairs={{0,2},{2,0},{4,6},{6,4},{1,3},{3,1},{5,7},{7,5}} | collective-permute-start | bytes 3538952 | tf_op jit(solution)/shard_map/ppermute | solution.py:27
  35.1 131.0 %collective-permute-start.14 = (bf16[384,1536]{1,0:T(8,128)(2,1)}, bf16[384,1536]{1,0:T(8,128)(2,1)}, u32[]{:S(2)}, u32[]{:S(2)}) collective-permute-start(bf16[384,1536]{1,0:T(8,128)(2,1)} %get-tuple-element.237), channel_id=1, source_target_pairs={{0,2},{2,0},{4,6},{6,4},{1,3},{3,1},{5,7},{7,5}} | collective-permute-start | bytes 3538952 | tf_op jit(solution)/shard_map/ppermute | solution.py:27
  38.3 129.3 %collective-permute-start = (bf16[512,1536]{1,0:T(8,128)(2,1)S(1)}, bf16[512,1536]{1,0:T(8,128)(2,1)}, u32[]{:S(2)}, u32[]{:S(2)}) collective-permute-start(bf16[512,1536]{1,0:T(8,128)(2,1)S(1)} %dynamic-slice_bitcast_fusion.2), channel_id=1, source_target_pairs={{0,1},{1,0},{2,3},{3,2},{4,5},{5,4},{6,7},{7,6}} | collective-permute-start | bytes 4718600 | tf_op jit(solution)/shard_map/ppermute | solution.py:35
  39.3 1455.6 %all-gather.10.cloned.1.call-start = ((), (), s32[]{:S(2)}) async-start(), calls=%async_computation.6 | async-start | bytes 14155776 | tf_op jit(solution)/shard_map/all_gather | solution.py:584
  76.6 93.4 %collective-permute-start.3 = (bf16[384,1536]{1,0:T(8,128)(2,1)}, bf16[384,1536]{1,0:T(8,128)(2,1)S(1)}, u32[]{:S(2)}, u32[]{:S(2)}) collective-permute-start(bf16[384,1536]{1,0:T(8,128)(2,1)} %collective-permute-done.2), channel_id=1, source_target_pairs={{0,1},{1,0},{2,3},{3,2},{4,5},{5,4},{6,7},{7,6}} | collective-permute-start | bytes 3538952 | tf_op jit(solution)/shard_map/ppermute | solution.py:35
  127.2 78.0 %collective-permute-start.16 = (bf16[384,1536]{1,0:T(8,128)(2,1)S(1)}, bf16[384,1536]{1,0:T(8,128)(2,1)S(1)}, u32[]{:S(2)}, u32[]{:S(2)}) collective-permute-start(bf16[384,1536]{1,0:T(8,128)(2,1)S(1)} %copy-done.29), channel_id=1, source_target_pairs={{0,2},{2,0},{4,6},{6,4},{1,3},{3,1},{5,7},{7,5}} | collective-permute-start | bytes 3538952 | tf_op jit(solution)/shard_map/ppermute | solution.py:27
  130.2 77.6 %collective-permute-start.8 = (bf16[384,1536]{1,0:T(8,128)(2,1)}, bf16[384,1536]{1,0:T(8,128)(2,1)S(1)}, u32[]{:S(2)}, u32[]{:S(2)}) collective-permute-start(bf16[384,1536]{1,0:T(8,128)(2,1)} %get-tuple-element.250), channel_id=1, source_target_pairs={{0,4},{4,0},{2,6},{6,2},{1,5},{5,1},{3,7},{7,3}} | collective-permute-start | bytes 3538952 | tf_op jit(solution)/shard_map/ppermute | solution.py:31
  166.1 43.2 %collective-permute-start.18 = (bf16[384,1536]{1,0:T(8,128)(2,1)}, bf16[384,1536]{1,0:T(8,128)(2,1)S(1)}, u32[]{:S(2)}, u32[]{:S(2)}) collective-permute-start(bf16[384,1536]{1,0:T(8,128)(2,1)} %get-tuple-element.237), channel_id=1, source_target_pairs={{0,4},{4,0},{2,6},{6,2},{1,5},{5,1},{3,7},{7,3}} | collective-permute-start | bytes 3538952 | tf_op jit(solution)/shard_map/ppermute | solution.py:31
  167.7 41.6 %collective-permute-start.15 = (bf16[384,1536]{1,0:T(8,128)(2,1)}, bf16[384,1536]{1,0:T(8,128)(2,1)S(1)}, u32[]{:S(2)}, u32[]{:S(2)}) collective-permute-start(bf16[384,1536]{1,0:T(8,128)(2,1)} %collective-permute-done.14), channel_id=1, source_target_pairs={{0,1},{1,0},{2,3},{3,2},{4,5},{5,4},{6,7},{7,6}} | collective-permute-start | bytes 3538952 | tf_op jit(solution)/shard_map/ppermute | solution.py:35
  170.1 42.0 %collective-permute-start.5 = (bf16[384,1536]{1,0:T(8,128)(2,1)}, bf16[384,1536]{1,0:T(8,128)(2,1)S(1)}, u32[]{:S(2)}, u32[]{:S(2)}) collective-permute-start(bf16[384,1536]{1,0:T(8,128)(2,1)} %collective-permute-done.4), channel_id=1, source_target_pairs={{0,1},{1,0},{2,3},{3,2},{4,5},{5,4},{6,7},{7,6}} | collective-permute-start | bytes 3538952 | tf_op jit(solution)/shard_map/ppermute | solution.py:35
  207.8 28.8 %collective-permute-start.20 = (bf16[384,1536]{1,0:T(8,128)(2,1)S(1)}, bf16[384,1536]{1,0:T(8,128)(2,1)S(1)}, u32[]{:S(2)}, u32[]{:S(2)}) collective-permute-start(bf16[384,1536]{1,0:T(8,128)(2,1)S(1)} %copy-done.29), channel_id=1, source_target_pairs={{0,4},{4,0},{2,6},{6,2},{1,5},{5,1},{3,7},{7,3}} | collective-permute-start | bytes 3538952 | tf_op jit(solution)/shard_map/ppermute | solution.py:31
  209.3 27.7 %collective-permute-start.7 = (bf16[384,1536]{1,0:T(8,128)(2,1)}, bf16[384,1536]{1,0:T(8,128)(2,1)S(1)}, u32[]{:S(2)}, u32[]{:S(2)}) collective-permute-start(bf16[384,1536]{1,0:T(8,128)(2,1)} %collective-permute-done.6), channel_id=1, source_target_pairs={{0,1},{1,0},{2,3},{3,2},{4,5},{5,4},{6,7},{7,6}} | collective-permute-start | bytes 3538952 | tf_op jit(solution)/shard_map/ppermute | solution.py:35
  209.3 29.3 %collective-permute-start.9 = (bf16[384,1536]{1,0:T(8,128)(2,1)S(1)}, bf16[384,1536]{1,0:T(8,128)(2,1)S(1)}, u32[]{:S(2)}, u32[]{:S(2)}) collective-permute-start(bf16[384,1536]{1,0:T(8,128)(2,1)S(1)} %collective-permute-done.8), channel_id=1, source_target_pairs={{0,1},{1,0},{2,3},{3,2},{4,5},{5,4},{6,7},{7,6}} | collective-permute-start | bytes 3538952 | tf_op jit(solution)/shard_map/ppermute | solution.py:35
  212.0 30.3 %collective-permute-start.19 = (bf16[384,1536]{1,0:T(8,128)(2,1)S(1)}, bf16[384,1536]{1,0:T(8,128)(2,1)S(1)}, u32[]{:S(2)}, u32[]{:S(2)}) collective-permute-start(bf16[384,1536]{1,0:T(8,128)(2,1)S(1)} %collective-permute-done.18), channel_id=1, source_target_pairs={{0,1},{1,0},{2,3},{3,2},{4,5},{5,4},{6,7},{7,6}} | collective-permute-start | bytes 3538952 | tf_op jit(solution)/shard_map/ppermute | solution.py:35
  215.6 46.3 %collective-permute-start.10 = (bf16[384,1536]{1,0:T(8,128)(2,1)}, bf16[384,1536]{1,0:T(8,128)(2,1)S(1)}, u32[]{:S(2)}, u32[]{:S(2)}) collective-permute-start(bf16[384,1536]{1,0:T(8,128)(2,1)} %collective-permute-done.2), channel_id=1, source_target_pairs={{0,4},{4,0},{2,6},{6,2},{1,5},{5,1},{3,7},{7,3}} | collective-permute-start | bytes 3538952 | tf_op jit(solution)/shard_map/ppermute | solution.py:31
  236.6 28.8 %collective-permute-start.12 = (bf16[384,1536]{1,0:T(8,128)(2,1)S(1)}, bf16[384,1536]{1,0:T(8,128)(2,1)S(1)}, u32[]{:S(2)}, u32[]{:S(2)}) collective-permute-start(bf16[384,1536]{1,0:T(8,128)(2,1)S(1)} %collective-permute-done.8), channel_id=1, source_target_pairs={{0,2},{2,0},{4,6},{6,4},{1,3},{3,1},{5,7},{7,5}} | collective-permute-start | bytes 3538952 | tf_op jit(solution)/shard_map/ppermute | solution.py:27
  236.9 49.7 %collective-permute-start.22 = (bf16[384,1536]{1,0:T(8,128)(2,1)}, bf16[384,1536]{1,0:T(8,128)(2,1)}, u32[]{:S(2)}, u32[]{:S(2)}) collective-permute-start(bf16[384,1536]{1,0:T(8,128)(2,1)} %collective-permute-done.14), channel_id=1, source_target_pairs={{0,4},{4,0},{2,6},{6,2},{1,5},{5,1},{3,7},{7,3}} | collective-permute-start | bytes 3538952 | tf_op jit(solution)/shard_map/ppermute | solution.py:31
  238.7 50.0 %collective-permute-start.24 = (bf16[384,1536]{1,0:T(8,128)(2,1)S(1)}, bf16[384,1536]{1,0:T(8,128)(2,1)}, u32[]{:S(2)}, u32[]{:S(2)}) collective-permute-start(bf16[384,1536]{1,0:T(8,128)(2,1)S(1)} %collective-permute-done.20), channel_id=1, source_target_pairs={{0,2},{2,0},{4,6},{6,4},{1,3},{3,1},{5,7},{7,5}} | collective-permute-start | bytes 3538952 | tf_op jit(solution)/shard_map/ppermute | solution.py:27
  242.3 48.6 %collective-permute-start.21 = (bf16[384,1536]{1,0:T(8,128)(2,1)S(1)}, bf16[384,1536]{1,0:T(8,128)(2,1)S(1)}, u32[]{:S(2)}, u32[]{:S(2)}) collective-permute-start(bf16[384,1536]{1,0:T(8,128)(2,1)S(1)} %collective-permute-done.20), channel_id=1, source_target_pairs={{0,1},{1,0},{2,3},{3,2},{4,5},{5,4},{6,7},{7,6}} | collective-permute-start | bytes 3538952 | tf_op jit(solution)/shard_map/ppermute | solution.py:35
  261.9 32.5 %collective-permute-start.11 = (bf16[384,1536]{1,0:T(8,128)(2,1)S(1)}, bf16[384,1536]{1,0:T(8,128)(2,1)S(1)}, u32[]{:S(2)}, u32[]{:S(2)}) collective-permute-start(bf16[384,1536]{1,0:T(8,128)(2,1)S(1)} %collective-permute-done.10), channel_id=1, source_target_pairs={{0,1},{1,0},{2,3},{3,2},{4,5},{5,4},{6,7},{7,6}} | collective-permute-start | bytes 3538952 | tf_op jit(solution)/shard_map/ppermute | solution.py:35
  265.4 65.2 %collective-permute-start.13 = (bf16[384,1536]{1,0:T(8,128)(2,1)S(1)}, bf16[384,1536]{1,0:T(8,128)(2,1)}, u32[]{:S(2)}, u32[]{:S(2)}) collective-permute-start(bf16[384,1536]{1,0:T(8,128)(2,1)S(1)} %collective-permute-done.12), channel_id=1, source_target_pairs={{0,1},{1,0},{2,3},{3,2},{4,5},{5,4},{6,7},{7,6}} | collective-permute-start | bytes 3538952 | tf_op jit(solution)/shard_map/ppermute | solution.py:35
  286.6 39.3 %collective-permute-start.23 = (bf16[384,1536]{1,0:T(8,128)(2,1)}, bf16[384,1536]{1,0:T(8,128)(2,1)}, u32[]{:S(2)}, u32[]{:S(2)}) collective-permute-start(bf16[384,1536]{1,0:T(8,128)(2,1)} %collective-permute-done.22), channel_id=1, source_target_pairs={{0,1},{1,0},{2,3},{3,2},{4,5},{5,4},{6,7},{7,6}} | collective-permute-start | bytes 3538952 | tf_op jit(solution)/shard_map/ppermute | solution.py:35
  288.7 44.3 %collective-permute-start.25 = (bf16[384,1536]{1,0:T(8,128)(2,1)}, bf16[384,1536]{1,0:T(8,128)(2,1)}, u32[]{:S(2)}, u32[]{:S(2)}) collective-permute-start(bf16[384,1536]{1,0:T(8,128)(2,1)} %collective-permute-done.24), channel_id=1, source_target_pairs={{0,1},{1,0},{2,3},{3,2},{4,5},{5,4},{6,7},{7,6}} | collective-permute-start | bytes 3538952 | tf_op jit(solution)/shard_map/ppermute | solution.py:35
  739.6 827.7 %all-gather.12.cloned.1.call-start = ((), (), s32[]{:S(2)}) async-start(), calls=%async_computation.7 | async-start | bytes 14155776 | tf_op jit(solution)/shard_map/all_gather | solution.py:584
  918.7 121.4 %all-to-all-start.3 = ((bf16[8,512,768]{2,1,0:T(8,128)(2,1)}), bf16[8,512,768]{2,1,0:T(8,128)(2,1)}, u32[]{:S(2)}, u32[]{:S(2)}) async-start(bf16[8,512,768]{2,1,0:T(8,128)(2,1)} %get-tuple-element.228), calls=%async_computation.3 | async-start | bytes 12582912 | tf_op jit(solution)/shard_map/all_to_all | solution.py:628
  1040.1 75.1 %all-to-all-start.1 = ((bf16[8,512,768]{2,1,0:T(8,128)(2,1)}), bf16[8,512,768]{2,1,0:T(8,128)(2,1)}, u32[]{:S(2)}, u32[]{:S(2)}) async-start(bf16[8,512,768]{2,1,0:T(8,128)(2,1)} %get-tuple-element.224), calls=%async_computation.1 | async-start | bytes 12582912 | tf_op jit(solution)/shard_map/all_to_all | solution.py:628
  1043.6 545.8 %all-gather.14.cloned.1.call-start = ((), (), s32[]{:S(2)}) async-start(), calls=%async_computation.8 | async-start | bytes 14155776 | tf_op jit(solution)/shard_map/all_gather | solution.py:584
  1108.0 190.0 %collective-permute-start.41 = (f32[2,512,1536]{2,1,0:T(8,128)}, f32[2,512,1536]{2,1,0:T(8,128)}, u32[]{:S(2)}, u32[]{:S(2)}) collective-permute-start(f32[2,512,1536]{2,1,0:T(8,128)} %get-tuple-element.196), channel_id=1, source_target_pairs={{0,1},{1,0},{2,3},{3,2},{4,5},{5,4},{6,7},{7,6}} | collective-permute-start | bytes 18874376 | tf_op jit(solution)/shard_map/ppermute | solution.py:35
  1115.1 223.2 %all-to-all-start = ((bf16[8,512,768]{2,1,0:T(8,128)(2,1)}), bf16[8,512,768]{2,1,0:T(8,128)(2,1)}, u32[]{:S(2)}, u32[]{:S(2)}) async-start(bf16[8,512,768]{2,1,0:T(8,128)(2,1)} %get-tuple-element.222), calls=%async_computation | async-start | bytes 12582912 | tf_op jit(solution)/shard_map/all_to_all | solution.py:628
  1119.4 167.7 %collective-permute-start.62 = (f32[2,384,768]{2,1,0:T(8,128)}, f32[2,384,768]{2,1,0:T(8,128)S(1)}, u32[]{:S(2)}, u32[]{:S(2)}) collective-permute-start(f32[2,384,768]{2,1,0:T(8,128)} %get-tuple-element.181), channel_id=1, source_target_pairs={{0,4},{4,0},{2,6},{6,2},{1,5},{5,1},{3,7},{7,3}} | collective-permute-start | bytes 7077896 | tf_op jit(solution)/shard_map/ppermute | solution.py:31
  1121.4 168.9 %collective-permute-start.59 = (f32[2,384,768]{2,1,0:T(8,128)}, f32[2,384,768]{2,1,0:T(8,128)S(1)}, u32[]{:S(2)}, u32[]{:S(2)}) collective-permute-start(f32[2,384,768]{2,1,0:T(8,128)} %get-tuple-element.180), channel_id=1, source_target_pairs={{0,2},{2,0},{4,6},{6,4},{1,3},{3,1},{5,7},{7,5}} | collective-permute-start | bytes 7077896 | tf_op jit(solution)/shard_map/ppermute | solution.py:27
  1122.9 214.9 %collective-permute-start.61 = (f32[2,384,768]{2,1,0:T(8,128)}, f32[2,384,768]{2,1,0:T(8,128)}, u32[]{:S(2)}, u32[]{:S(2)}) collective-permute-start(f32[2,384,768]{2,1,0:T(8,128)} %get-tuple-element.189), channel_id=1, source_target_pairs={{0,4},{4,0},{2,6},{6,2},{1,5},{5,1},{3,7},{7,3}} | collective-permute-start | bytes 7077896 | tf_op jit(solution)/shard_map/ppermute | solution.py:31
  1123.4 214.4 %collective-permute-start.58 = (f32[2,384,768]{2,1,0:T(8,128)}, f32[2,384,768]{2,1,0:T(8,128)}, u32[]{:S(2)}, u32[]{:S(2)}) collective-permute-start(f32[2,384,768]{2,1,0:T(8,128)} %get-tuple-element.178), channel_id=1, source_target_pairs={{0,2},{2,0},{4,6},{6,4},{1,3},{3,1},{5,7},{7,5}} | collective-permute-start | bytes 7077896 | tf_op jit(solution)/shard_map/ppermute | solution.py:27
  1288.8 99.0 %collective-permute-start.63 = (f32[2,384,768]{2,1,0:T(8,128)}, f32[2,384,768]{2,1,0:T(8,128)}, u32[]{:S(2)}, u32[]{:S(2)}) collective-permute-start(f32[2,384,768]{2,1,0:T(8,128)} %add.350), channel_id=1, source_target_pairs={{0,2},{2,0},{4,6},{6,4},{1,3},{3,1},{5,7},{7,5}} | collective-permute-start | bytes 7077896 | tf_op jit(solution)/shard_map/ppermute | solution.py:27
  1292.0 96.4 %collective-permute-start.60 = (f32[2,384,768]{2,1,0:T(8,128)}, f32[2,384,768]{2,1,0:T(8,128)}, u32[]{:S(2)}, u32[]{:S(2)}) collective-permute-start(f32[2,384,768]{2,1,0:T(8,128)} %add.347), channel_id=1, source_target_pairs={{0,4},{4,0},{2,6},{6,2},{1,5},{5,1},{3,7},{7,3}} | collective-permute-start | bytes 7077896 | tf_op jit(solution)/shard_map/ppermute | solution.py:31
  1331.9 76.1 %collective-permute-start.42 = (f32[2,384,768]{2,1,0:T(8,128)}, f32[2,384,768]{2,1,0:T(8,128)S(1)}, u32[]{:S(2)}, u32[]{:S(2)}) collective-permute-start(f32[2,384,768]{2,1,0:T(8,128)} %get-tuple-element.198), channel_id=1, source_target_pairs={{0,1},{1,0},{2,3},{3,2},{4,5},{5,4},{6,7},{7,6}} | collective-permute-start | bytes 7077896 | tf_op jit(solution)/shard_map/ppermute | solution.py:35
  1337.8 70.4 %collective-permute-start.43 = (f32[2,384,768]{2,1,0:T(8,128)}, f32[2,384,768]{2,1,0:T(8,128)}, u32[]{:S(2)}, u32[]{:S(2)}) collective-permute-start(f32[2,384,768]{2,1,0:T(8,128)} %get-tuple-element.199), channel_id=1, source_target_pairs={{0,1},{1,0},{2,3},{3,2},{4,5},{5,4},{6,7},{7,6}} | collective-permute-start | bytes 7077896 | tf_op jit(solution)/shard_map/ppermute | solution.py:35
  1337.8 70.7 %collective-permute-start.44 = (f32[2,384,768]{2,1,0:T(8,128)}, f32[2,384,768]{2,1,0:T(8,128)}, u32[]{:S(2)}, u32[]{:S(2)}) collective-permute-start(f32[2,384,768]{2,1,0:T(8,128)} %get-tuple-element.200), channel_id=1, source_target_pairs={{0,1},{1,0},{2,3},{3,2},{4,5},{5,4},{6,7},{7,6}} | collective-permute-start | bytes 7077896 | tf_op jit(solution)/shard_map/ppermute | solution.py:35
  1338.3 146.6 %all-to-all-start.2 = ((bf16[8,512,768]{2,1,0:T(8,128)(2,1)}), bf16[8,512,768]{2,1,0:T(8,128)(2,1)}, u32[]{:S(2)}, u32[]{:S(2)}) async-start(bf16[8,512,768]{2,1,0:T(8,128)(2,1)} %get-tuple-element.226), calls=%async_computation.2 | async-start | bytes 12582912 | tf_op jit(solution)/shard_map/all_to_all | solution.py:628
  1388.3 29.9 %collective-permute-start.45 = (f32[2,384,768]{2,1,0:T(8,128)}, f32[2,384,768]{2,1,0:T(8,128)}, u32[]{:S(2)}, u32[]{:S(2)}) collective-permute-start(f32[2,384,768]{2,1,0:T(8,128)} %get-tuple-element.201), channel_id=1, source_target_pairs={{0,1},{1,0},{2,3},{3,2},{4,5},{5,4},{6,7},{7,6}} | collective-permute-start | bytes 7077896 | tf_op jit(solution)/shard_map/ppermute | solution.py:35
  1407.6 34.9 %collective-permute-start.46 = (f32[2,384,768]{2,1,0:T(8,128)}, f32[2,384,768]{2,1,0:T(8,128)}, u32[]{:S(2)}, u32[]{:S(2)}) collective-permute-start(f32[2,384,768]{2,1,0:T(8,128)} %get-tuple-element.208), channel_id=1, source_target_pairs={{0,1},{1,0},{2,3},{3,2},{4,5},{5,4},{6,7},{7,6}} | collective-permute-start | bytes 7077896 | tf_op jit(solution)/shard_map/ppermute | solution.py:35
  1408.0 35.0 %collective-permute-start.47 = (f32[2,384,768]{2,1,0:T(8,128)}, f32[2,384,768]{2,1,0:T(8,128)}, u32[]{:S(2)}, u32[]{:S(2)}) collective-permute-start(f32[2,384,768]{2,1,0:T(8,128)} %get-tuple-element.209), channel_id=1, source_target_pairs={{0,1},{1,0},{2,3},{3,2},{4,5},{5,4},{6,7},{7,6}} | collective-permute-start | bytes 7077896 | tf_op jit(solution)/shard_map/ppermute | solution.py:35
  1408.2 34.9 %collective-permute-start.48 = (f32[2,384,768]{2,1,0:T(8,128)}, f32[2,384,768]{2,1,0:T(8,128)}, u32[]{:S(2)}, u32[]{:S(2)}) collective-permute-start(f32[2,384,768]{2,1,0:T(8,128)} %get-tuple-element.210), channel_id=1, source_target_pairs={{0,1},{1,0},{2,3},{3,2},{4,5},{5,4},{6,7},{7,6}} | collective-permute-start | bytes 7077896 | tf_op jit(solution)/shard_map/ppermute | solution.py:35
  1408.5 54.8 %collective-permute-start.49 = (f32[2,384,768]{2,1,0:T(8,128)}, f32[2,384,768]{2,1,0:T(8,128)}, u32[]{:S(2)}, u32[]{:S(2)}) collective-permute-start(f32[2,384,768]{2,1,0:T(8,128)} %get-tuple-element.211), channel_id=1, source_target_pairs={{0,1},{1,0},{2,3},{3,2},{4,5},{5,4},{6,7},{7,6}} | collective-permute-start | bytes 7077896 | tf_op jit(solution)/shard_map/ppermute | solution.py:35
  1418.2 93.1 %collective-permute-start.66 = (bf16[2048,1536]{1,0:T(8,128)(2,1)}, bf16[2048,1536]{1,0:T(8,128)(2,1)}, u32[]{:S(2)}, u32[]{:S(2)}) collective-permute-start(bf16[2048,1536]{1,0:T(8,128)(2,1)} %bitcast.28), channel_id=1, source_target_pairs={{0,1},{1,0},{2,3},{3,2},{4,5},{5,4},{6,7},{7,6}} | collective-permute-start | bytes 18874376 | tf_op jit(solution)/shard_map/ppermute | solution.py:35
  1442.6 141.2 %collective-permute-start.65 = (f32[768,768]{1,0:T(8,128)}, f32[768,768]{1,0:T(8,128)}, u32[]{:S(2)}, u32[]{:S(2)}) collective-permute-start(f32[768,768]{1,0:T(8,128)} %bitcast.26.ob_ref), channel_id=1, source_target_pairs={{0,1},{1,0},{2,3},{3,2},{4,5},{5,4},{6,7},{7,6}} | collective-permute-start | bytes 7077896 | tf_op jit(solution)/shard_map/ppermute | solution.py:35
  1443.1 145.6 %collective-permute-start.64 = (f32[768,768]{1,0:T(8,128)}, f32[768,768]{1,0:T(8,128)}, u32[]{:S(2)}, u32[]{:S(2)}) collective-permute-start(f32[768,768]{1,0:T(8,128)} %bitcast.25.oa_ref), channel_id=1, source_target_pairs={{0,1},{1,0},{2,3},{3,2},{4,5},{5,4},{6,7},{7,6}} | collective-permute-start | bytes 7077896 | tf_op jit(solution)/shard_map/ppermute | solution.py:35
  1443.1 78.6 %collective-permute-start.71 = (bf16[512,1536]{1,0:T(8,128)(2,1)S(1)}, bf16[512,1536]{1,0:T(8,128)(2,1)}, u32[]{:S(2)}, u32[]{:S(2)}) collective-permute-start(bf16[512,1536]{1,0:T(8,128)(2,1)S(1)} %get-tuple-element.247), channel_id=1, source_target_pairs={{0,2},{2,0},{5,7},{7,5}} | collective-permute-start | bytes 4718600 | tf_op jit(solution)/shard_map/ppermute | solution.py:670
  1463.3 66.7 %collective-permute-start.54 = (f32[2,384,768]{2,1,0:T(8,128)}, f32[2,384,768]{2,1,0:T(8,128)}, u32[]{:S(2)}, u32[]{:S(2)}) collective-permute-start(f32[2,384,768]{2,1,0:T(8,128)} %get-tuple-element.203), channel_id=1, source_target_pairs={{0,4},{4,0},{2,6},{6,2},{1,5},{5,1},{3,7},{7,3}} | collective-permute-start | bytes 7077896 | tf_op jit(solution)/shard_map/ppermute | solution.py:31
  1511.3 53.7 %collective-permute-start.51 = (f32[2,384,768]{2,1,0:T(8,128)S(1)}, f32[2,384,768]{2,1,0:T(8,128)S(1)}, u32[]{:S(2)}, u32[]{:S(2)}) collective-permute-start(f32[2,384,768]{2,1,0:T(8,128)S(1)} %copy-done.31), channel_id=1, source_target_pairs={{0,2},{2,0},{4,6},{6,4},{1,3},{3,1},{5,7},{7,5}} | collective-permute-start | bytes 7077896 | tf_op jit(solution)/shard_map/ppermute | solution.py:27
  1521.7 67.6 %collective-permute-start.69 = (bf16[512,1536]{1,0:T(8,128)(2,1)}, bf16[512,1536]{1,0:T(8,128)(2,1)}, u32[]{:S(2)}, u32[]{:S(2)}) collective-permute-start(bf16[512,1536]{1,0:T(8,128)(2,1)} %get-tuple-element.246), channel_id=1, source_target_pairs={{0,4},{2,6},{5,1},{7,3}} | collective-permute-start | bytes 4718600 | tf_op jit(solution)/shard_map/ppermute | solution.py:669
  1530.0 81.0 %collective-permute-start.53 = (f32[2,384,768]{2,1,0:T(8,128)}, f32[2,384,768]{2,1,0:T(8,128)}, u32[]{:S(2)}, u32[]{:S(2)}) collective-permute-start(f32[2,384,768]{2,1,0:T(8,128)} %get-tuple-element.215), channel_id=1, source_target_pairs={{0,4},{4,0},{2,6},{6,2},{1,5},{5,1},{3,7},{7,3}} | collective-permute-start | bytes 7077896 | tf_op jit(solution)/shard_map/ppermute | solution.py:31
  1565.0 116.5 %collective-permute-start.50 = (f32[2,384,768]{2,1,0:T(8,128)}, f32[2,384,768]{2,1,0:T(8,128)}, u32[]{:S(2)}, u32[]{:S(2)}) collective-permute-start(f32[2,384,768]{2,1,0:T(8,128)} %get-tuple-element.204), channel_id=1, source_target_pairs={{0,2},{2,0},{4,6},{6,4},{1,3},{3,1},{5,7},{7,5}} | collective-permute-start | bytes 7077896 | tf_op jit(solution)/shard_map/ppermute | solution.py:27
  1583.8 122.7 %collective-permute-start.72 = (bf16[1024,1536]{1,0:T(8,128)(2,1)}, bf16[1024,1536]{1,0:T(8,128)(2,1)}, u32[]{:S(2)}, u32[]{:S(2)}) collective-permute-start(bf16[1024,1536]{1,0:T(8,128)(2,1)} %pad_maximum_fusion.3), channel_id=1, source_target_pairs={{0,4},{2,6},{5,1},{7,3}} | collective-permute-start | bytes 9437192 | tf_op jit(solution)/shard_map/ppermute | solution.py:674
  1588.7 80.1 %collective-permute-start.55 = (f32[2,384,768]{2,1,0:T(8,128)}, f32[2,384,768]{2,1,0:T(8,128)}, u32[]{:S(2)}, u32[]{:S(2)}) collective-permute-start(f32[2,384,768]{2,1,0:T(8,128)} %add.344), channel_id=1, source_target_pairs={{0,2},{2,0},{4,6},{6,4},{1,3},{3,1},{5,7},{7,5}} | collective-permute-start | bytes 7077896 | tf_op jit(solution)/shard_map/ppermute | solution.py:27
  1589.3 92.2 %collective-permute-start.52 = (f32[2,384,768]{2,1,0:T(8,128)}, f32[2,384,768]{2,1,0:T(8,128)}, u32[]{:S(2)}, u32[]{:S(2)}) collective-permute-start(f32[2,384,768]{2,1,0:T(8,128)} %add.341), channel_id=1, source_target_pairs={{0,4},{4,0},{2,6},{6,2},{1,5},{5,1},{3,7},{7,3}} | collective-permute-start | bytes 7077896 | tf_op jit(solution)/shard_map/ppermute | solution.py:31
  1611.0 109.5 %collective-permute-start.67 = (f32[768,1536]{1,0:T(8,128)}, f32[768,1536]{1,0:T(8,128)}, u32[]{:S(2)}, u32[]{:S(2)}) collective-permute-start(f32[768,1536]{1,0:T(8,128)} %add_add_fusion.refs_0_), channel_id=1, source_target_pairs={{0,1},{1,0},{2,3},{3,2},{4,5},{5,4},{6,7},{7,6}} | collective-permute-start | bytes 14155784 | tf_op jit(solution)/shard_map/ppermute | solution.py:35
  1668.8 35.6 %collective-permute-start.70 = (bf16[512,1536]{1,0:T(8,128)(2,1)}, bf16[512,1536]{1,0:T(8,128)(2,1)}, u32[]{:S(2)}, u32[]{:S(2)}) collective-permute-start(bf16[512,1536]{1,0:T(8,128)(2,1)} %broadcast_select_fusion.3), channel_id=1, source_target_pairs={{0,2},{2,0},{4,6},{6,4},{1,3},{3,1},{5,7},{7,5}} | collective-permute-start | bytes 4718600 | tf_op jit(solution)/shard_map/ppermute | solution.py:27
  1681.5 29.0 %collective-permute-start.57 = (f32[2,384,768]{2,1,0:T(8,128)S(1)}, f32[2,384,768]{2,1,0:T(8,128)S(1)}, u32[]{:S(2)}, u32[]{:S(2)}) collective-permute-start(f32[2,384,768]{2,1,0:T(8,128)S(1)} %add_add_fusion.3.own_b), channel_id=1, source_target_pairs={{0,1},{1,0},{2,3},{3,2},{4,5},{5,4},{6,7},{7,6}} | collective-permute-start | bytes 7077896 | tf_op jit(solution)/shard_map/ppermute | solution.py:35
  1685.2 26.8 %collective-permute-start.56 = (f32[2,384,768]{2,1,0:T(8,128)S(1)}, f32[2,384,768]{2,1,0:T(8,128)}, u32[]{:S(2)}, u32[]{:S(2)}) collective-permute-start(f32[2,384,768]{2,1,0:T(8,128)S(1)} %add_add_fusion.4.own_a), channel_id=1, source_target_pairs={{0,1},{1,0},{2,3},{3,2},{4,5},{5,4},{6,7},{7,6}} | collective-permute-start | bytes 7077896 | tf_op jit(solution)/shard_map/ppermute | solution.py:35
  (54 other events, 2267.4 us)
Sparse Core Ops, SparseCore 0:
  16.2 129.7 all-gather.5
  148.4 52.1 all-gather.7
  739.7 66.6 all-gather.9
  841.2 66.4 all-gather.11
  1108.5 147.9 all-gather.13

commit v9 on v8

--- a/solution.py
+++ b/solution.py
@@ -57,6 +57,7 @@
 
 
 CHUNK = 256
+WIDE = 256
 
 
 def masked_pair(q):
@@ -67,65 +68,69 @@
 
 def attn_fwd_body(*refs):
     q_ref, qn_ref, ko_ref, ks_ref, kno_ref, kns_ref, vo_ref, vs_ref = refs[:8]
-    ctx_ref, lse_ref, a_ref, b_ref, ma_ref, mb_ref = refs[-6:]
-
-    def scores(ko, ks, q, s_ref, m_ref):
-        s = nt(jnp.concatenate([ko[...], ks[...]], axis=0), masked_pair(q))
-        s_ref[...] = s
-        m_ref[...] = jnp.max(s, axis=0, keepdims=True)
-
-    def finish(s_ref, m_ref, i):
-        rows = slice(i * CHUNK, (i + 1) * CHUNK)
-        m = m_ref[...]
-        p = jnp.exp2((s_ref[...] - m) * (SCALE * LOG2E))
+    ctx_ref, lse_ref, a_ref, ma_ref = refs[-4:]
+    units = [(sub, i) for sub in range(WIDE // 128) for i in range(q_ref.shape[0] // CHUNK)]
+
+    def joined(own_ref, sib_ref, sub):
+        cols = slice(sub * 128, (sub + 1) * 128)
+        return jnp.concatenate([own_ref[:, cols], sib_ref[:, cols]], axis=0)
+
+    def scores(ko, ks, q, sub, i):
+        s = nt(joined(ko, ks, sub), masked_pair(q[i * CHUNK:(i + 1) * CHUNK, sub * 128:(sub + 1) * 128]))
+        return s, jnp.max(s, axis=0, keepdims=True)
+
+    @pl.when(pl.program_id(0) == 0)
+    def _():
+        a_ref[...], ma_ref[...] = scores(ko_ref, ks_ref, q_ref, 0, 0)
+
+    s, m = a_ref[...], ma_ref[...]
+    for n, (sub, i) in enumerate(units):
+        if n + 1 < len(units):
+            ahead = scores(ko_ref, ks_ref, q_ref, *units[n + 1])
+        else:
+            ahead = scores(kno_ref, kns_ref, qn_ref, 0, 0)
+        rows, cols = slice(i * CHUNK, (i + 1) * CHUNK), slice(sub * 128, (sub + 1) * 128)
+        p = jnp.exp2((s - m) * (SCALE * LOG2E))
         l = jnp.sum(p, axis=0, keepdims=True)
         pb = (p * (1.0 / l)).astype(BF16)
         lse = m * (SCALE * LOG2E) + jnp.log2(l)
-        lse_ref[0, 0:1, rows] = lse[:, :CHUNK]
-        lse_ref[0, 1:2, rows] = lse[:, CHUNK:]
-        ctx_t = tn(jnp.concatenate([vo_ref[...], vs_ref[...]], axis=0), pb)
+        lse_ref[sub, 0:1, rows] = lse[:, :CHUNK]
+        lse_ref[sub, 1:2, rows] = lse[:, CHUNK:]
+        ctx_t = tn(joined(vo_ref, vs_ref, sub), pb)
         ctx_t = jnp.concatenate([ctx_t[:HEAD_DIM, :CHUNK], ctx_t[HEAD_DIM:, CHUNK:]], axis=0)
-        ctx_ref[0, 0, rows, :] = ctx_t.T.astype(BF16)
-
-    @pl.when(pl.program_id(0) == 0)
-    def _():
-        scores(ko_ref, ks_ref, q_ref[:CHUNK, :], a_ref, ma_ref)
-
-    scores(ko_ref, ks_ref, q_ref[CHUNK:, :], b_ref, mb_ref)
-    finish(a_ref, ma_ref, 0)
-    scores(kno_ref, kns_ref, qn_ref[:CHUNK, :], a_ref, ma_ref)
-    finish(b_ref, mb_ref, 1)
+        ctx_ref[0, 0, rows, cols] = ctx_t.T.astype(BF16)
+        s, m = ahead
+    a_ref[...], ma_ref[...] = s, m
 
 
 def attn_fwd(q, kv, kv_s, layer, layers, hist):
     tq, width = q.shape
     tk = kv.shape[0]
     pairs = width // 128
-    last = pairs - 1
+    steps = width // WIDE
 
     def col(off):
         return lambda j: (0, j + off)
 
     def nxt(j):
-        return (0, jnp.minimum(j + 1, last))
+        return (0, jnp.minimum(j + 1, steps - 1))
 
     extra = [] if hist is None else [hist]
     flops = 2 * 2 * tq * (2 * tk) * 256 * (width // HEAD_DIM)
     return pl.pallas_call(
         attn_fwd_body,
-        grid=(pairs,),
-        in_specs=[pl.BlockSpec((tq, 128), col(0)), pl.BlockSpec((tq, 128), nxt),
-                  pl.BlockSpec((tk, 128), col(0)), pl.BlockSpec((tk, 128), col(0)),
-                  pl.BlockSpec((tk, 128), nxt), pl.BlockSpec((tk, 128), nxt),
-                  pl.BlockSpec((tk, 128), col(pairs)), pl.BlockSpec((tk, 128), col(pairs))]
+        grid=(steps,),
+        in_specs=[pl.BlockSpec((tq, WIDE), col(0)), pl.BlockSpec((tq, WIDE), nxt),
+                  pl.BlockSpec((tk, WIDE), col(0)), pl.BlockSpec((tk, WIDE), col(0)),
+                  pl.BlockSpec((tk, WIDE), nxt), pl.BlockSpec((tk, WIDE), nxt),
+                  pl.BlockSpec((tk, WIDE), col(steps)), pl.BlockSpec((tk, WIDE), col(steps))]
         + [pl.BlockSpec(memory_space=pl.ANY)] * len(extra),
-        out_specs=[pl.BlockSpec((1, 1, tq, 128), lambda j: (3, layer, 0, j)),
-                   pl.BlockSpec((1, 2, tq), lambda j: (j, 0, 0))],
+        out_specs=[pl.BlockSpec((1, 1, tq, WIDE), lambda j: (3, layer, 0, j)),
+                   pl.BlockSpec((WIDE // 128, 2, tq), lambda j: (j, 0, 0))],
         out_shape=[jax.ShapeDtypeStruct((4, layers, tq, width), BF16),
                    jax.ShapeDtypeStruct((pairs, 2, tq), F32)],
         input_output_aliases={8: 0} if extra else {},
-        scratch_shapes=[pltpu.VMEM((2 * tk, 2 * CHUNK), F32), pltpu.VMEM((2 * tk, 2 * CHUNK), F32),
-                        pltpu.VMEM((1, 2 * CHUNK), F32), pltpu.VMEM((1, 2 * CHUNK), F32)],
+        scratch_shapes=[pltpu.VMEM((2 * tk, 2 * CHUNK), F32), pltpu.VMEM((1, 2 * CHUNK), F32)],
         compiler_params=pltpu.CompilerParams(dimension_semantics=('arbitrary',),
                                              vmem_limit_bytes=VMEM_ALL),
         cost_estimate=pl.CostEstimate(flops=flops, bytes_accessed=2 * (tq * width * 2 + 4 * tk * width),
@@ -134,40 +139,46 @@
     )(q, q, kv, kv_s, kv, kv_s, kv, kv_s, *extra)
 
 
-WIDE = 256
-
-
 def attn_bwd_body(q_ref, ko_ref, ks_ref, vo_ref, vs_ref, do_ref, lse_ref, hist_ref, dq_ref, down_ref, dsib_ref):
     tk = ko_ref.shape[0]
     low = pair_masks(CHUNK)
-    for sub in range(WIDE // 128):
+    units = [(sub, i, h) for sub in range(WIDE // 128) for i in range(q_ref.shape[0] // CHUNK) for h in range(2)]
+
+    def keys(own_ref, sib_ref, sub):
         cols = slice(sub * 128, (sub + 1) * 128)
-        k = jnp.concatenate([ko_ref[:, cols], ks_ref[:, cols]], axis=0)
-        v = jnp.concatenate([vo_ref[:, cols], vs_ref[:, cols]], axis=0)
-        for i in range(q_ref.shape[0] // CHUNK):
-            rows = slice(i * CHUNK, (i + 1) * CHUNK)
-            q = q_ref[rows, cols]
-            do = do_ref[rows, cols]
+        return jnp.concatenate([own_ref[:, cols], sib_ref[:, cols]], axis=0)
+
+    def masked(ref, sub, i, h):
+        v = ref[i * CHUNK:(i + 1) * CHUNK, sub * 128:(sub + 1) * 128]
+        return jnp.where(low if h == 0 else ~low, v, jnp.zeros_like(v))
+
+    def products(sub, i, h):
+        s = nt(keys(ko_ref, ks_ref, sub), masked(q_ref, sub, i, h))
+        return s, nt(keys(vo_ref, vs_ref, sub), masked(do_ref, sub, i, h)).astype(BF16)
+
+    dqs = []
+    ahead = products(*units[0])
+    for n, (sub, i, h) in enumerate(units):
+        s, dp = ahead
+        if n + 1 < len(units):
+            ahead = products(*units[n + 1])
+        rows, cols = slice(i * CHUNK, (i + 1) * CHUNK), slice(sub * 128, (sub + 1) * 128)
+        p = jnp.exp2(s * (SCALE * LOG2E) - lse_ref[sub, h:h + 1, rows])
+        dp = dp.astype(F32)
+        delta = jnp.sum(p * dp, axis=0, keepdims=True)
+        ds = (p * (dp - delta)).astype(BF16)
+        dv = nn(p.astype(BF16), masked(do_ref, sub, i, h))
+        dk = nn(ds, masked(q_ref, sub, i, h) * jnp.asarray(SCALE, BF16))
+        for m, grad in enumerate((dk, dv)):
+            for ref, part in ((down_ref, grad[:tk]), (dsib_ref, grad[tk:])):
+                if i == 0 and h == 0:
+                    ref[m, :, cols] = part
+                else:
+                    ref[m, :, cols] += part
+        dqs.append(tn(keys(ko_ref, ks_ref, sub), ds)[h * HEAD_DIM:(h + 1) * HEAD_DIM, :] * SCALE)
+        if h == 1:
+            dq_ref[0, 0, rows, cols] = jnp.concatenate(dqs, axis=0).T.astype(BF16)
             dqs = []
-            for h in range(2):
-                sel = low if h == 0 else ~low
-                qm = jnp.where(sel, q, jnp.zeros_like(q))
-                dom = jnp.where(sel, do, jnp.zeros_like(do))
-                s = nt(k, qm)
-                p = jnp.exp2(s * (SCALE * LOG2E) - lse_ref[sub, h:h + 1, rows])
-                dp = nt(v, dom).astype(BF16).astype(F32)
-                delta = jnp.sum(p * dp, axis=0, keepdims=True)
-                ds = (p * (dp - delta)).astype(BF16)
-                dv = nn(p.astype(BF16), dom)
-                dk = nn(ds, qm) * SCALE
-                for n, grad in enumerate((dk, dv)):
-                    for ref, part in ((down_ref, grad[:tk]), (dsib_ref, grad[tk:])):
-                        if i == 0 and h == 0:
-                            ref[n, :, cols] = part
-                        else:
-                            ref[n, :, cols] += part
-                dqs.append(tn(k, ds)[h * HEAD_DIM:(h + 1) * HEAD_DIM, :] * SCALE)
-            dq_ref[0, 0, rows, cols] = jnp.concatenate(dqs, axis=0).T.astype(BF16)
 
 
 def attn_bwd(q, kv, kv_s, d_ctx, lse, layer, layers, hist):
@@ -487,7 +498,7 @@
     size = sum(v.size for v in own)
     return pl.pallas_call(
         body,
-        grid_spec=pltpu.PrefetchScalarGridSpec(num_scalar_prefetch=1, grid=grid, in_specs=in_specs * 2, out_specs=out_specs),
+        grid_spec=pltpu.PrefetchScalarGridSpec(num_scalar_prefetch=1, grid=grid, in_specs=in_specs, out_specs=out_specs),
         out_shape=out_shape,
         compiler_params=pltpu.CompilerParams(dimension_semantics=('arbitrary', 'arbitrary'), vmem_limit_bytes=VMEM_ALL),
         cost_estimate=pl.CostEstimate(flops=8 * size, bytes_accessed=16 * size, transcendentals=0),
@@ -496,8 +507,9 @@
 
 def join(core, own, other):
     rows, cols = own.shape[0] // 4, own.shape[1]
-    block = pl.BlockSpec((rows, cols), lambda i, j, c: (j, 0))
-    return join_call(core, functools.partial(join_body, 1), (2, 4), [own], [other], [block],
+    first = pl.BlockSpec((rows, cols), lambda i, j, c: (jnp.where(i == 0, j, 3), 0))
+    then = pl.BlockSpec((rows, cols), lambda i, j, c: (jnp.where(i == 0, 0, j), 0))
+    return join_call(core, functools.partial(join_body, 1), (2, 4), [own], [other], [first, then],
                      pl.BlockSpec((rows, cols), lambda i, j, c: (4 * ((c[0] + i) % 2) + j, 0)),
                      jax.ShapeDtypeStruct((8 * rows, cols), F32))
 
@@ -517,7 +529,7 @@
     block = pl.BlockSpec((2, hid, half_d), lambda i, j, c: (0, 0, 0))
     tall = pl.BlockSpec((half_d, hid), lambda i, j, c: ((c[0] + i) % 2, 0))
     wide = pl.BlockSpec((hid, half_d), lambda i, j, c: (0, (c[0] + i) % 2))
-    return join_call(core, join_attn_body, (2, 1), list(own), list(other), [block] * 2, [tall] * 3 + [wide],
+    return join_call(core, join_attn_body, (2, 1), list(own), list(other), [block] * 4, [tall] * 3 + [wide],
                      [jax.ShapeDtypeStruct((2 * half_d, hid), F32)] * 3 + [jax.ShapeDtypeStruct((hid, 2 * half_d), F32)])
 
 
@@ -532,7 +544,7 @@
 def join_flip(core, own, other):
     rows, cols = own[0].shape
     block = pl.BlockSpec((rows, cols), lambda i, j, c: (0, 0))
-    return join_call(core, join_flip_body, (2, 2), own, other, [block] * 2,
+    return join_call(core, join_flip_body, (2, 2), own, other, [block] * 4,
                      pl.BlockSpec((cols, rows), lambda i, j, c: (j, (c[0] + i) % 2)),
                      jax.ShapeDtypeStruct((2 * cols, 2 * rows), F32))
 

time: 1750 us -> 1700 us (0.971)
  Pallas kernels: 825 us -> 791 us
    pallas_call x4, Pallas kernels: 168 us -> 144 us  [attn_bwd(): pl.pallas_call(attn_bwd_body, grid=(steps,), in_specs=[qblk, kblk, kblk,...]
    ppermute x1, starting transfers between devices: 20.2 us -> 2.5 us  [device_step(): q_x = lax.ppermute(part_q, BOTH, in_row)]
  transfers between devices with their start and end apart: 82 -> 82, of which waited for: 23 -> 23; matrix products, arithmetic and copies ran while one was open for 16% -> 16% of each run, Pallas kernels for 27% -> 26%
where the time goes in v9:
time: 1700 us; the launch traced here: 1690 us
  Pallas kernels  791 us (47%)
  waiting for transfers between devices  539 us (32%)
  matrix products  125 us (7%)
  local copies, waits for them, and re-layouts  109 us (6%)
  starting transfers between devices  61.4 us (4%)
  other arithmetic  52.7 us (3%)
    ppermute x13, waiting for transfers between devices, pp_x(): return lax.ppermute(v, 'model', SWAP_X)  284 us
    ppermute x12, waiting for transfers between devices, pp_y(): return lax.ppermute(v, 'model', SWAP_Y)  223 us
    pallas_call x8, Pallas kernels, terms(): pl.pallas_call(functools.partial(terms_body, len(recv) // 4, slot_of), gr...  163 us
    pallas_call x4, Pallas kernels, attn_bwd(): pl.pallas_call(attn_bwd_body, grid=(steps,), in_specs=[qblk, kblk, kblk,...  144 us
    pallas_call x4, Pallas kernels, mlp_bwd(): pl.pallas_call(mlp_bwd_body, grid=(hidden // BLOCK_B,), in_specs=[whole,...  137 us
    pallas_call x4, Pallas kernels, mlp_fwd(): pl.pallas_call(mlp_fwd_body, grid=(hidden // BLOCK_F,), in_specs=[whole,...  134 us
    dot_general x13, matrix products, dot(): return lax.dot_general(a, b, (dims, ((), ())), preferred_element_type=F32)  125 us
    pallas_call x4, Pallas kernels, attn_fwd(): pl.pallas_call(attn_fwd_body, grid=(steps,), in_specs=[pl.BlockSpec((tq,...  86.8 us
  transfers between devices with their start and end apart: 82, of which 23 were waited for; matrix products, arithmetic and copies ran while one was open for 16% of the time, Pallas kernels for 26%

profile of v9, /device:TPU:0, one launch (start us, length us, event | category | flops | bytes accessed | tf_op | source)
XLA Modules:
  0.0 1691.4 jit_solution(15088062196598703117)
XLA Ops:
  16.2 6.6 copy.43
  39.8 7.3 broadcast.6.clone
  50.2 26.4 %collective-permute-done.2 = bf16[384,1536]{1,0:T(8,128)(2,1)} collective-permute-done((bf16[384,1536]{1,0:T(8,128)(2,1)}, bf16[384,1536]{1,0:T(8,128)(2,1)}, u32[]{:S(2)}, u32[]{:S(2)}) %collective-permute-start.2) | collective-permute-done | bytes 1179680 | tf_op jit(solution)/shard_map/ppermute | solution.py:27
  77.1 6.5 broadcast.6.clone.1
  86.1 41.1 %collective-permute-done.4 = bf16[384,1536]{1,0:T(8,128)(2,1)} collective-permute-done((bf16[384,1536]{1,0:T(8,128)(2,1)}, bf16[384,1536]{1,0:T(8,128)(2,1)}, u32[]{:S(2)}, u32[]{:S(2)}) %collective-permute-start.4) | collective-permute-done | bytes 1179680 | tf_op jit(solution)/shard_map/ppermute | solution.py:27
  131.8 34.3 %collective-permute-done.14 = bf16[384,1536]{1,0:T(8,128)(2,1)} collective-permute-done((bf16[384,1536]{1,0:T(8,128)(2,1)}, bf16[384,1536]{1,0:T(8,128)(2,1)}, u32[]{:S(2)}, u32[]{:S(2)}) %collective-permute-start.14) | collective-permute-done | bytes 1179680 | tf_op jit(solution)/shard_map/ppermute | solution.py:27
  175.3 29.9 %collective-permute-done.16 = bf16[384,1536]{1,0:T(8,128)(2,1)S(1)} collective-permute-done((bf16[384,1536]{1,0:T(8,128)(2,1)S(1)}, bf16[384,1536]{1,0:T(8,128)(2,1)S(1)}, u32[]{:S(2)}, u32[]{:S(2)}) %collective-permute-start.16) | collective-permute-done | bytes 1179680 | tf_op jit(solution)/shard_map/ppermute | solution.py:27
  217.1 19.4 %collective-permute-done.20 = bf16[384,1536]{1,0:T(8,128)(2,1)S(1)} collective-permute-done((bf16[384,1536]{1,0:T(8,128)(2,1)S(1)}, bf16[384,1536]{1,0:T(8,128)(2,1)S(1)}, u32[]{:S(2)}, u32[]{:S(2)}) %collective-permute-start.20) | collective-permute-done | bytes 1179680 | tf_op jit(solution)/shard_map/ppermute | solution.py:31
  244.5 17.3 %collective-permute-done.10 = bf16[384,1536]{1,0:T(8,128)(2,1)S(1)} collective-permute-done((bf16[384,1536]{1,0:T(8,128)(2,1)}, bf16[384,1536]{1,0:T(8,128)(2,1)S(1)}, u32[]{:S(2)}, u32[]{:S(2)}) %collective-permute-start.10) | collective-permute-done | bytes 1179680 | tf_op jit(solution)/shard_map/ppermute | solution.py:31
  265.4 21.2 %collective-permute-done.22 = bf16[384,1536]{1,0:T(8,128)(2,1)} collective-permute-done((bf16[384,1536]{1,0:T(8,128)(2,1)}, bf16[384,1536]{1,0:T(8,128)(2,1)}, u32[]{:S(2)}, u32[]{:S(2)}) %collective-permute-start.22) | collective-permute-done | bytes 1179680 | tf_op jit(solution)/shard_map/ppermute | solution.py:31
  313.5 10.8 norm_kv.4
  340.9 7.7 convolution_convert_fusion.3.refs_0_.refs_1_.q_ref
  348.6 21.7 %attn_fwd.4 = (bf16[4,4,512,1536]{3,2,1,0:T(8,128)(2,1)}, f32[12,2,512]{2,1,0:T(2,128)}) custom-call(bf16[512,1536]{1,0:T(8,128)(2,1)} %convolution_convert_fusion.3.refs_0_.refs_1_.q_ref, bf16[512,1536]{1,0:T(8,128)(2,1)} %convolution_convert_fusion.3.refs_0_.refs_1_.q_ref, bf16[512,3072]{1,0:T(8,128)(2,1)} %get-tuple-element.120.refs_2_.refs_4_.refs_6_.ko_ref.vo_ref, ...), custom_call_target="tpu_custom_call" | custom-call | flops 12884901888 | bytes 9437184 | tf_op jit(solution)/shard_map/attn_fwd/pallas_call | solution.py:120
  370.3 33.6 %mlp_fwd.4 = (bf16[512,6144]{1,0:T(8,128)(2,1)}, bf16[8,512,768]{2,1,0:T(8,128)(2,1)}, bf16[512,1536]{1,0:T(8,128)(2,1)}, bf16[512,1536]{1,0:T(8,128)(2,1)}, bf16[4,512,1536]{2,1,0:T(8,128)(2,1)}) custom-call(bf16[512,1536]{1,0:T(8,128)(2,1)} %bitcast_select_fusion.1.refs_0_.x_hbm, f32[1,1536]{1,0:T(1,128)} %get-tuple-element.255.refs_1_.e_ref, ...), custom_call_target="tpu_custom_call" | custom-call | flops 19327352832 | bytes 50331648 | tf_op jit(solution)/shard_map/mlp_fwd/pallas_call | solution.py:400
  403.9 10.1 norm_kv.5
  420.0 21.7 %attn_fwd.5 = (bf16[4,4,512,1536]{3,2,1,0:T(8,128)(2,1)}, f32[12,2,512]{2,1,0:T(2,128)}) custom-call(bf16[512,1536]{1,0:T(8,128)(2,1)} %convolution_convert_fusion.2.refs_0_.refs_1_.q_ref, bf16[512,1536]{1,0:T(8,128)(2,1)} %convolution_convert_fusion.2.refs_0_.refs_1_.q_ref, ...), custom_call_target="tpu_custom_call", output_to_operand_aliasing={{0}: (8, {})} | custom-call | flops 12884901888 | bytes 9437184 | tf_op jit(solution)/shard_map/attn_fwd/pallas_call | solution.py:120
  441.7 33.6 %mlp_fwd.5 = (bf16[512,6144]{1,0:T(8,128)(2,1)}, bf16[8,512,768]{2,1,0:T(8,128)(2,1)}, bf16[512,1536]{1,0:T(8,128)(2,1)}, bf16[512,1536]{1,0:T(8,128)(2,1)}, bf16[4,512,1536]{2,1,0:T(8,128)(2,1)}) custom-call(bf16[512,1536]{1,0:T(8,128)(2,1)} %get-tuple-element.122.refs_0_.x_hbm, ...), custom_call_target="tpu_custom_call", output_to_operand_aliasing={{4}: (6, {})} | custom-call | flops 19327352832 | bytes 50331648 | tf_op jit(solution)/shard_map/mlp_fwd/pallas_call | solution.py:400
  475.3 9.9 norm_kv.6
  485.3 5.6 convolution_convert_fusion.1.refs_0_.refs_1_.q_ref
  491.2 21.9 %attn_fwd.6 = (bf16[4,4,512,1536]{3,2,1,0:T(8,128)(2,1)}, f32[12,2,512]{2,1,0:T(2,128)}) custom-call(bf16[512,1536]{1,0:T(8,128)(2,1)} %convolution_convert_fusion.1.refs_0_.refs_1_.q_ref, bf16[512,1536]{1,0:T(8,128)(2,1)} %convolution_convert_fusion.1.refs_0_.refs_1_.q_ref, ...), custom_call_target="tpu_custom_call", output_to_operand_aliasing={{0}: (8, {})} | custom-call | flops 12884901888 | bytes 9437184 | tf_op jit(solution)/shard_map/attn_fwd/pallas_call | solution.py:120
  513.1 33.6 %mlp_fwd.6 = (bf16[512,6144]{1,0:T(8,128)(2,1)}, bf16[8,512,768]{2,1,0:T(8,128)(2,1)}, bf16[512,1536]{1,0:T(8,128)(2,1)}, bf16[512,1536]{1,0:T(8,128)(2,1)}, bf16[4,512,1536]{2,1,0:T(8,128)(2,1)}) custom-call(bf16[512,1536]{1,0:T(8,128)(2,1)} %get-tuple-element.127.refs_0_.x_hbm, ...), custom_call_target="tpu_custom_call", output_to_operand_aliasing={{4}: (6, {})} | custom-call | flops 19327352832 | bytes 50331648 | tf_op jit(solution)/shard_map/mlp_fwd/pallas_call | solution.py:400
  546.7 10.0 norm_kv.7
  558.9 5.8 collective-permute-done.29
  567.8 7.9 convolution_convert_fusion.refs_0_.refs_1_.q_ref
  575.7 21.5 %attn_fwd.7 = (bf16[4,4,512,1536]{3,2,1,0:T(8,128)(2,1)}, f32[12,2,512]{2,1,0:T(2,128)}) custom-call(bf16[512,1536]{1,0:T(8,128)(2,1)} %convolution_convert_fusion.refs_0_.refs_1_.q_ref, bf16[512,1536]{1,0:T(8,128)(2,1)} %convolution_convert_fusion.refs_0_.refs_1_.q_ref, ...), custom_call_target="tpu_custom_call", output_to_operand_aliasing={{0}: (8, {})} | custom-call | flops 12884901888 | bytes 9437184 | tf_op jit(solution)/shard_map/attn_fwd/pallas_call | solution.py:120
  597.3 33.5 %mlp_fwd.7 = (bf16[512,6144]{1,0:T(8,128)(2,1)}, bf16[8,512,768]{2,1,0:T(8,128)(2,1)}, bf16[512,1536]{1,0:T(8,128)(2,1)}, bf16[512,1536]{1,0:T(8,128)(2,1)}, bf16[4,512,1536]{2,1,0:T(8,128)(2,1)}) custom-call(bf16[512,1536]{1,0:T(8,128)(2,1)} %get-tuple-element.132.refs_0_.x_hbm, ...), custom_call_target="tpu_custom_call", output_to_operand_aliasing={{4}: (6, {})} | custom-call | flops 19327352832 | bytes 50331648 | tf_op jit(solution)/shard_map/mlp_fwd/pallas_call | solution.py:400
  630.8 34.4 %mlp_bwd.4 = (bf16[4,512,6144]{2,1,0:T(8,128)(2,1)}, bf16[2,4,512,1536]{3,2,1,0:T(8,128)(2,1)}, bf16[512,1536]{1,0:T(8,128)(2,1)}) custom-call(bf16[512,1536]{1,0:T(8,128)(2,1)} %bitcast_select_fusion.refs_0_, bf16[512,1536]{1,0:T(8,128)(2,1)} %get-tuple-element.137.refs_1_, ...), custom_call_target="tpu_custom_call", output_to_operand_aliasing={{1}: (6, {})} | custom-call | flops 19327352832 | bytes 50331648 | tf_op jit(solution)/shard_map/mlp_bwd/pallas_call | solution.py:470
  665.2 36.0 %attn_bwd.4 = (bf16[4,4,512,1536]{3,2,1,0:T(8,128)(2,1)}, f32[2,512,1536]{2,1,0:T(8,128)}, f32[2,512,1536]{2,1,0:T(8,128)}) custom-call(bf16[512,1536]{1,0:T(8,128)(2,1)} %convolution_convert_fusion.refs_0_.refs_1_.q_ref, bf16[512,3072]{1,0:T(8,128)(2,1)} %get-tuple-element.134.refs_2_.refs_4_.refs_6_.ko_ref.vo_ref, ...), custom_call_target="tpu_custom_call", output_to_operand_aliasing={{0}: (7, {})} | custom-call | flops 32212254720 | bytes 25165824 | tf_op jit(solution)/shard_map/attn_bwd/pallas_call | solution.py:197
  701.3 6.0 fusion.13.acc0_hbm
  711.7 14.4 d_kv.4
  726.2 34.2 %mlp_bwd.5 = (bf16[4,512,6144]{2,1,0:T(8,128)(2,1)}, bf16[2,4,512,1536]{3,2,1,0:T(8,128)(2,1)}, bf16[512,1536]{1,0:T(8,128)(2,1)}) custom-call(bf16[512,1536]{1,0:T(8,128)(2,1)} %get-tuple-element.145.refs_0_, bf16[512,1536]{1,0:T(8,128)(2,1)} %get-tuple-element.146.refs_1_, ...), custom_call_target="tpu_custom_call", output_to_operand_aliasing={{1}: (6, {}), {0}: (7, {})} | custom-call | flops 19327352832 | bytes 50331648 | tf_op jit(solution)/shard_map/mlp_bwd/pallas_call | solution.py:470
  760.4 36.2 %attn_bwd.5 = (bf16[4,4,512,1536]{3,2,1,0:T(8,128)(2,1)}, f32[2,512,1536]{2,1,0:T(8,128)}, f32[2,512,1536]{2,1,0:T(8,128)}) custom-call(bf16[512,1536]{1,0:T(8,128)(2,1)} %convolution_convert_fusion.1.refs_0_.refs_1_.q_ref, bf16[512,3072]{1,0:T(8,128)(2,1)} %get-tuple-element.129.refs_2_.refs_4_.refs_6_.ko_ref.vo_ref, ...), custom_call_target="tpu_custom_call", output_to_operand_aliasing={{0}: (7, {})} | custom-call | flops 32212254720 | bytes 25165824 | tf_op jit(solution)/shard_map/attn_bwd/pallas_call | solution.py:197
  796.7 6.0 fusion.11.acc0_hbm
  807.2 14.5 d_kv.5
  821.7 34.3 %mlp_bwd.6 = (bf16[4,512,6144]{2,1,0:T(8,128)(2,1)}, bf16[2,4,512,1536]{3,2,1,0:T(8,128)(2,1)}, bf16[512,1536]{1,0:T(8,128)(2,1)}) custom-call(bf16[512,1536]{1,0:T(8,128)(2,1)} %get-tuple-element.156.refs_0_, bf16[512,1536]{1,0:T(8,128)(2,1)} %get-tuple-element.157.refs_1_, ...), custom_call_target="tpu_custom_call", output_to_operand_aliasing={{1}: (6, {}), {0}: (7, {})} | custom-call | flops 19327352832 | bytes 50331648 | tf_op jit(solution)/shard_map/mlp_bwd/pallas_call | solution.py:470
  856.0 35.9 %attn_bwd.6 = (bf16[4,4,512,1536]{3,2,1,0:T(8,128)(2,1)}, f32[2,512,1536]{2,1,0:T(8,128)}, f32[2,512,1536]{2,1,0:T(8,128)}) custom-call(bf16[512,1536]{1,0:T(8,128)(2,1)} %convolution_convert_fusion.2.refs_0_.refs_1_.q_ref, bf16[512,3072]{1,0:T(8,128)(2,1)} %get-tuple-element.124.refs_2_.refs_4_.refs_6_.ko_ref.vo_ref, ...), custom_call_target="tpu_custom_call", output_to_operand_aliasing={{0}: (7, {})} | custom-call | flops 32212254720 | bytes 25165824 | tf_op jit(solution)/shard_map/attn_bwd/pallas_call | solution.py:197
  896.3 6.0 fusion.9.acc0_hbm
  902.4 14.6 d_kv.6
  917.0 34.1 %mlp_bwd.7 = (bf16[4,512,6144]{2,1,0:T(8,128)(2,1)}, bf16[2,4,512,1536]{3,2,1,0:T(8,128)(2,1)}, bf16[512,1536]{1,0:T(8,128)(2,1)}) custom-call(bf16[512,1536]{1,0:T(8,128)(2,1)} %get-tuple-element.167.refs_0_, bf16[512,1536]{1,0:T(8,128)(2,1)} %get-tuple-element.168.refs_1_, ...), custom_call_target="tpu_custom_call", output_to_operand_aliasing={{1}: (6, {}), {0}: (7, {})} | custom-call | flops 19327352832 | bytes 50331648 | tf_op jit(solution)/shard_map/mlp_bwd/pallas_call | solution.py:470
  951.1 19.5 %shard_map.144 = (f32[2,384,768]{2,1,0:T(8,128)}, f32[2,384,768]{2,1,0:T(8,128)}, f32[2,384,768]{2,1,0:T(8,128)}, f32[2,384,768]{2,1,0:T(8,128)}) custom-call(s32[5]{0:T(128)} %stack.32.places_ref, bf16[1,2048,6144]{2,1,0:T(8,128)(2,1)} %bitcast.72, bf16[1,2048,1536]{2,1,0:T(8,128)(2,1)} %bitcast.76), custom_call_target="tpu_custom_call" | custom-call | flops 9663676416 | bytes 18874368 | tf_op jit(solution)/shard_map/pallas_call | solution.py:315
  971.6 19.7 %shard_map.146 = (f32[2,384,768]{2,1,0:T(8,128)}, f32[2,384,768]{2,1,0:T(8,128)}, f32[2,384,768]{2,1,0:T(8,128)}, f32[2,384,768]{2,1,0:T(8,128)}) custom-call(s32[5]{0:T(128)} %stack.32.places_ref, bf16[1,2048,6144]{2,1,0:T(8,128)(2,1)} %bitcast.73, bf16[1,2048,1536]{2,1,0:T(8,128)(2,1)} %bitcast.77), custom_call_target="tpu_custom_call" | custom-call | flops 9663676416 | bytes 18874368 | tf_op jit(solution)/shard_map/pallas_call | solution.py:315
  992.9 21.1 %shard_map.145 = (f32[2,384,768]{2,1,0:T(8,128)}, f32[2,384,768]{2,1,0:T(8,128)}, f32[2,384,768]{2,1,0:T(8,128)}, f32[2,384,768]{2,1,0:T(8,128)}) custom-call(s32[5]{0:T(128)} %stack.30.places_ref, bf16[1,2048,6144]{2,1,0:T(8,128)(2,1)} %bitcast.74, bf16[1,2048,1536]{2,1,0:T(8,128)(2,1)} %bitcast.78, f32[2,384,768]{2,1,0:T(8,128)} %collective-permute-done.33.refs_0_, ...), custom_call_target="tpu_custom_call" | custom-call | flops 9663676416 | bytes 18874368 | tf_op jit(solution)/shard_map/pallas_call | solution.py:315
  1018.9 21.1 %shard_map.147 = (f32[2,384,768]{2,1,0:T(8,128)}, f32[2,384,768]{2,1,0:T(8,128)}, f32[2,384,768]{2,1,0:T(8,128)}, f32[2,384,768]{2,1,0:T(8,128)}) custom-call(s32[5]{0:T(128)} %stack.30.places_ref, bf16[1,2048,6144]{2,1,0:T(8,128)(2,1)} %bitcast.75, bf16[1,2048,1536]{2,1,0:T(8,128)(2,1)} %bitcast.79, f32[2,384,768]{2,1,0:T(8,128)} %copy-done.17, ...), custom_call_target="tpu_custom_call" | custom-call | flops 9663676416 | bytes 18874368 | tf_op jit(solution)/shard_map/pallas_call | solution.py:315
  1040.1 35.7 %attn_bwd.7 = (bf16[4,4,512,1536]{3,2,1,0:T(8,128)(2,1)}, f32[2,512,1536]{2,1,0:T(8,128)}, f32[2,512,1536]{2,1,0:T(8,128)}) custom-call(bf16[512,1536]{1,0:T(8,128)(2,1)} %convolution_convert_fusion.3.refs_0_.refs_1_.q_ref, bf16[512,3072]{1,0:T(8,128)(2,1)} %get-tuple-element.120.refs_2_.refs_4_.refs_6_.ko_ref.vo_ref, ...), custom_call_target="tpu_custom_call", output_to_operand_aliasing={{0}: (7, {})} | custom-call | flops 32212254720 | bytes 25165824 | tf_op jit(solution)/shard_map/attn_bwd/pallas_call | solution.py:197
  1076.2 15.6 all-to-all-done.1
  1100.0 157.7 %collective-permute-done.62 = f32[2,384,768]{2,1,0:T(8,128)S(1)} collective-permute-done((f32[2,384,768]{2,1,0:T(8,128)}, f32[2,384,768]{2,1,0:T(8,128)S(1)}, u32[]{:S(2)}, u32[]{:S(2)}) %collective-permute-start.62) | collective-permute-done | bytes 2359328 | tf_op jit(solution)/shard_map/ppermute | solution.py:31
  1268.0 14.7 d_kv.7
  1282.6 19.2 %shard_map.148 = (f32[2,384,768]{2,1,0:T(8,128)}, f32[2,384,768]{2,1,0:T(8,128)}, f32[2,384,768]{2,1,0:T(8,128)}, f32[2,384,768]{2,1,0:T(8,128)}) custom-call(s32[5]{0:T(128)} %stack.32.places_ref, bf16[4,2048,1536]{2,1,0:T(8,128)(2,1)} %bitcast.64, bf16[2,2048,1536]{2,1,0:T(8,128)(2,1)} %bitcast.68), custom_call_target="tpu_custom_call" | custom-call | flops 9663676416 | bytes 18874368 | tf_op jit(solution)/shard_map/pallas_call | solution.py:315
  1301.9 6.4 collective-permute-done.61
  1312.3 45.6 %collective-permute-done.63 = f32[2,384,768]{2,1,0:T(8,128)} collective-permute-done((f32[2,384,768]{2,1,0:T(8,128)}, f32[2,384,768]{2,1,0:T(8,128)}, u32[]{:S(2)}, u32[]{:S(2)}) %collective-permute-start.63) | collective-permute-done | bytes 2359328 | tf_op jit(solution)/shard_map/ppermute | solution.py:27
  1358.9 19.3 %shard_map.150 = (f32[2,384,768]{2,1,0:T(8,128)}, f32[2,384,768]{2,1,0:T(8,128)}, f32[2,384,768]{2,1,0:T(8,128)}, f32[2,384,768]{2,1,0:T(8,128)}) custom-call(s32[5]{0:T(128)} %stack.32.places_ref, bf16[4,2048,1536]{2,1,0:T(8,128)(2,1)} %bitcast.65, bf16[2,2048,1536]{2,1,0:T(8,128)(2,1)} %bitcast.69), custom_call_target="tpu_custom_call" | custom-call | flops 9663676416 | bytes 18874368 | tf_op jit(solution)/shard_map/pallas_call | solution.py:315
  1391.8 21.3 %shard_map.149 = (f32[2,384,768]{2,1,0:T(8,128)}, f32[2,384,768]{2,1,0:T(8,128)}, f32[2,384,768]{2,1,0:T(8,128)}, f32[2,384,768]{2,1,0:T(8,128)}) custom-call(s32[5]{0:T(128)} %stack.30.places_ref, bf16[4,2048,1536]{2,1,0:T(8,128)(2,1)} %bitcast.66, bf16[2,2048,1536]{2,1,0:T(8,128)(2,1)} %bitcast.70, f32[2,384,768]{2,1,0:T(8,128)} %copy-done.9, ...), custom_call_target="tpu_custom_call" | custom-call | flops 9663676416 | bytes 18874368 | tf_op jit(solution)/shard_map/pallas_call | solution.py:315
  1416.5 21.5 %shard_map.151 = (f32[2,384,768]{2,1,0:T(8,128)}, f32[2,384,768]{2,1,0:T(8,128)}, f32[2,384,768]{2,1,0:T(8,128)}, f32[2,384,768]{2,1,0:T(8,128)}) custom-call(s32[5]{0:T(128)} %stack.30.places_ref, bf16[4,2048,1536]{2,1,0:T(8,128)(2,1)} %bitcast.67, bf16[2,2048,1536]{2,1,0:T(8,128)(2,1)} %bitcast.71, f32[2,384,768]{2,1,0:T(8,128)} %collective-permute-done.46.refs_0_, ...), custom_call_target="tpu_custom_call" | custom-call | flops 9663676416 | bytes 18874368 | tf_op jit(solution)/shard_map/pallas_call | solution.py:315
  1438.0 10.0 fusion.2
  1448.0 16.4 fusion.32
  1465.6 10.0 fusion
  1489.0 29.3 %collective-permute-done.51 = f32[2,384,768]{2,1,0:T(8,128)S(1)} collective-permute-done((f32[2,384,768]{2,1,0:T(8,128)S(1)}, f32[2,384,768]{2,1,0:T(8,128)S(1)}, u32[]{:S(2)}, u32[]{:S(2)}) %collective-permute-start.51) | collective-permute-done | bytes 2359328 | tf_op jit(solution)/shard_map/ppermute | solution.py:27
  1521.5 16.5 fusion.33
  1543.0 21.6 %add_add_fusion.refs_0_ = f32[768,1536]{1,0:T(8,128)} fusion(f32[768,1536]{1,0:T(8,128)} %fusion.33, f32[768,1536]{1,0:T(8,128)} %fusion.32, f32[768,1536]{1,0:T(8,128)} %fusion.2, f32[768,1536]{1,0:T(8,128)} %fusion, bf16[4096,768]{1,0:T(8,128)(2,1)} %bitcast.31, bf16[4096,1536]{1,0:T(8,128)(2,1)} %all-gather.14.cloned.1.call-done), kind=kOutput, calls=%fused_computation.4 | convolution fusion | flops 9668395008 | bytes 42467328 | tf_op jit(solution)/shard_map/dot_general | solution.py:39
  1567.6 54.7 %collective-permute-done.55 = f32[2,384,768]{2,1,0:T(8,128)} collective-permute-done((f32[2,384,768]{2,1,0:T(8,128)}, f32[2,384,768]{2,1,0:T(8,128)}, u32[]{:S(2)}, u32[]{:S(2)}) %collective-permute-start.55) | collective-permute-done | bytes 2359328 | tf_op jit(solution)/shard_map/ppermute | solution.py:27
  1624.0 8.7 shard_map.153
  1640.1 18.2 %collective-permute-done.70 = bf16[512,1536]{1,0:T(8,128)(2,1)} collective-permute-done((bf16[512,1536]{1,0:T(8,128)(2,1)}, bf16[512,1536]{1,0:T(8,128)(2,1)}, u32[]{:S(2)}, u32[]{:S(2)}) %collective-permute-start.70) | collective-permute-done | bytes 1572896 | tf_op jit(solution)/shard_map/ppermute | solution.py:27
  1665.9 8.5 shard_map.152
  1674.4 10.2 shard_map.154
  (297 shorter events, 228.8 us)
Async XLA Ops:
  7.2 288.3 %all-gather.6.cloned.1.call-start = ((), (), s32[]{:S(2)}) async-start(), calls=%async_computation.4 | async-start | bytes 15925248 | tf_op jit(solution)/shard_map/all_gather | solution.py:596
  16.1 319.3 %all-gather.8.cloned.1.call-start = ((), (), s32[]{:S(2)}) async-start(), calls=%async_computation.5 | async-start | bytes 5308416 | tf_op jit(solution)/shard_map/all_gather | solution.py:596
  26.5 50.1 %collective-permute-start.2 = (bf16[384,1536]{1,0:T(8,128)(2,1)}, bf16[384,1536]{1,0:T(8,128)(2,1)}, u32[]{:S(2)}, u32[]{:S(2)}) collective-permute-start(bf16[384,1536]{1,0:T(8,128)(2,1)} %get-tuple-element.251), channel_id=1, source_target_pairs={{0,2},{2,0},{4,6},{6,4},{1,3},{3,1},{5,7},{7,5}} | collective-permute-start | bytes 3538952 | tf_op jit(solution)/shard_map/ppermute | solution.py:27
  29.9 100.3 %collective-permute-start.6 = (bf16[384,1536]{1,0:T(8,128)(2,1)}, bf16[384,1536]{1,0:T(8,128)(2,1)}, u32[]{:S(2)}, u32[]{:S(2)}) collective-permute-start(bf16[384,1536]{1,0:T(8,128)(2,1)} %get-tuple-element.251), channel_id=1, source_target_pairs={{0,4},{4,0},{2,6},{6,2},{1,5},{5,1},{3,7},{7,3}} | collective-permute-start | bytes 3538952 | tf_op jit(solution)/shard_map/ppermute | solution.py:31
  31.4 95.8 %collective-permute-start.4 = (bf16[384,1536]{1,0:T(8,128)(2,1)}, bf16[384,1536]{1,0:T(8,128)(2,1)}, u32[]{:S(2)}, u32[]{:S(2)}) collective-permute-start(bf16[384,1536]{1,0:T(8,128)(2,1)} %get-tuple-element.250), channel_id=1, source_target_pairs={{0,2},{2,0},{4,6},{6,4},{1,3},{3,1},{5,7},{7,5}} | collective-permute-start | bytes 3538952 | tf_op jit(solution)/shard_map/ppermute | solution.py:27
  35.1 131.0 %collective-permute-start.14 = (bf16[384,1536]{1,0:T(8,128)(2,1)}, bf16[384,1536]{1,0:T(8,128)(2,1)}, u32[]{:S(2)}, u32[]{:S(2)}) collective-permute-start(bf16[384,1536]{1,0:T(8,128)(2,1)} %get-tuple-element.237), channel_id=1, source_target_pairs={{0,2},{2,0},{4,6},{6,4},{1,3},{3,1},{5,7},{7,5}} | collective-permute-start | bytes 3538952 | tf_op jit(solution)/shard_map/ppermute | solution.py:27
  38.3 129.3 %collective-permute-start = (bf16[512,1536]{1,0:T(8,128)(2,1)S(1)}, bf16[512,1536]{1,0:T(8,128)(2,1)}, u32[]{:S(2)}, u32[]{:S(2)}) collective-permute-start(bf16[512,1536]{1,0:T(8,128)(2,1)S(1)} %dynamic-slice_bitcast_fusion.2), channel_id=1, source_target_pairs={{0,1},{1,0},{2,3},{3,2},{4,5},{5,4},{6,7},{7,6}} | collective-permute-start | bytes 4718600 | tf_op jit(solution)/shard_map/ppermute | solution.py:35
  39.3 1408.7 %all-gather.10.cloned.1.call-start = ((), (), s32[]{:S(2)}) async-start(), calls=%async_computation.6 | async-start | bytes 14155776 | tf_op jit(solution)/shard_map/all_gather | solution.py:596
  76.6 93.4 %collective-permute-start.3 = (bf16[384,1536]{1,0:T(8,128)(2,1)}, bf16[384,1536]{1,0:T(8,128)(2,1)S(1)}, u32[]{:S(2)}, u32[]{:S(2)}) collective-permute-start(bf16[384,1536]{1,0:T(8,128)(2,1)} %collective-permute-done.2), channel_id=1, source_target_pairs={{0,1},{1,0},{2,3},{3,2},{4,5},{5,4},{6,7},{7,6}} | collective-permute-start | bytes 3538952 | tf_op jit(solution)/shard_map/ppermute | solution.py:35
  127.2 78.0 %collective-permute-start.16 = (bf16[384,1536]{1,0:T(8,128)(2,1)S(1)}, bf16[384,1536]{1,0:T(8,128)(2,1)S(1)}, u32[]{:S(2)}, u32[]{:S(2)}) collective-permute-start(bf16[384,1536]{1,0:T(8,128)(2,1)S(1)} %copy-done.29), channel_id=1, source_target_pairs={{0,2},{2,0},{4,6},{6,4},{1,3},{3,1},{5,7},{7,5}} | collective-permute-start | bytes 3538952 | tf_op jit(solution)/shard_map/ppermute | solution.py:27
  130.2 77.6 %collective-permute-start.8 = (bf16[384,1536]{1,0:T(8,128)(2,1)}, bf16[384,1536]{1,0:T(8,128)(2,1)S(1)}, u32[]{:S(2)}, u32[]{:S(2)}) collective-permute-start(bf16[384,1536]{1,0:T(8,128)(2,1)} %get-tuple-element.250), channel_id=1, source_target_pairs={{0,4},{4,0},{2,6},{6,2},{1,5},{5,1},{3,7},{7,3}} | collective-permute-start | bytes 3538952 | tf_op jit(solution)/shard_map/ppermute | solution.py:31
  166.1 43.2 %collective-permute-start.18 = (bf16[384,1536]{1,0:T(8,128)(2,1)}, bf16[384,1536]{1,0:T(8,128)(2,1)S(1)}, u32[]{:S(2)}, u32[]{:S(2)}) collective-permute-start(bf16[384,1536]{1,0:T(8,128)(2,1)} %get-tuple-element.237), channel_id=1, source_target_pairs={{0,4},{4,0},{2,6},{6,2},{1,5},{5,1},{3,7},{7,3}} | collective-permute-start | bytes 3538952 | tf_op jit(solution)/shard_map/ppermute | solution.py:31
  167.7 41.6 %collective-permute-start.15 = (bf16[384,1536]{1,0:T(8,128)(2,1)}, bf16[384,1536]{1,0:T(8,128)(2,1)S(1)}, u32[]{:S(2)}, u32[]{:S(2)}) collective-permute-start(bf16[384,1536]{1,0:T(8,128)(2,1)} %collective-permute-done.14), channel_id=1, source_target_pairs={{0,1},{1,0},{2,3},{3,2},{4,5},{5,4},{6,7},{7,6}} | collective-permute-start | bytes 3538952 | tf_op jit(solution)/shard_map/ppermute | solution.py:35
  170.1 42.0 %collective-permute-start.5 = (bf16[384,1536]{1,0:T(8,128)(2,1)}, bf16[384,1536]{1,0:T(8,128)(2,1)S(1)}, u32[]{:S(2)}, u32[]{:S(2)}) collective-permute-start(bf16[384,1536]{1,0:T(8,128)(2,1)} %collective-permute-done.4), channel_id=1, source_target_pairs={{0,1},{1,0},{2,3},{3,2},{4,5},{5,4},{6,7},{7,6}} | collective-permute-start | bytes 3538952 | tf_op jit(solution)/shard_map/ppermute | solution.py:35
  207.8 28.8 %collective-permute-start.20 = (bf16[384,1536]{1,0:T(8,128)(2,1)S(1)}, bf16[384,1536]{1,0:T(8,128)(2,1)S(1)}, u32[]{:S(2)}, u32[]{:S(2)}) collective-permute-start(bf16[384,1536]{1,0:T(8,128)(2,1)S(1)} %copy-done.29), channel_id=1, source_target_pairs={{0,4},{4,0},{2,6},{6,2},{1,5},{5,1},{3,7},{7,3}} | collective-permute-start | bytes 3538952 | tf_op jit(solution)/shard_map/ppermute | solution.py:31
  209.3 27.7 %collective-permute-start.7 = (bf16[384,1536]{1,0:T(8,128)(2,1)}, bf16[384,1536]{1,0:T(8,128)(2,1)S(1)}, u32[]{:S(2)}, u32[]{:S(2)}) collective-permute-start(bf16[384,1536]{1,0:T(8,128)(2,1)} %collective-permute-done.6), channel_id=1, source_target_pairs={{0,1},{1,0},{2,3},{3,2},{4,5},{5,4},{6,7},{7,6}} | collective-permute-start | bytes 3538952 | tf_op jit(solution)/shard_map/ppermute | solution.py:35
  209.3 29.3 %collective-permute-start.9 = (bf16[384,1536]{1,0:T(8,128)(2,1)S(1)}, bf16[384,1536]{1,0:T(8,128)(2,1)S(1)}, u32[]{:S(2)}, u32[]{:S(2)}) collective-permute-start(bf16[384,1536]{1,0:T(8,128)(2,1)S(1)} %collective-permute-done.8), channel_id=1, source_target_pairs={{0,1},{1,0},{2,3},{3,2},{4,5},{5,4},{6,7},{7,6}} | collective-permute-start | bytes 3538952 | tf_op jit(solution)/shard_map/ppermute | solution.py:35
  212.0 30.3 %collective-permute-start.19 = (bf16[384,1536]{1,0:T(8,128)(2,1)S(1)}, bf16[384,1536]{1,0:T(8,128)(2,1)S(1)}, u32[]{:S(2)}, u32[]{:S(2)}) collective-permute-start(bf16[384,1536]{1,0:T(8,128)(2,1)S(1)} %collective-permute-done.18), channel_id=1, source_target_pairs={{0,1},{1,0},{2,3},{3,2},{4,5},{5,4},{6,7},{7,6}} | collective-permute-start | bytes 3538952 | tf_op jit(solution)/shard_map/ppermute | solution.py:35
  215.6 46.3 %collective-permute-start.10 = (bf16[384,1536]{1,0:T(8,128)(2,1)}, bf16[384,1536]{1,0:T(8,128)(2,1)S(1)}, u32[]{:S(2)}, u32[]{:S(2)}) collective-permute-start(bf16[384,1536]{1,0:T(8,128)(2,1)} %collective-permute-done.2), channel_id=1, source_target_pairs={{0,4},{4,0},{2,6},{6,2},{1,5},{5,1},{3,7},{7,3}} | collective-permute-start | bytes 3538952 | tf_op jit(solution)/shard_map/ppermute | solution.py:31
  236.6 28.8 %collective-permute-start.12 = (bf16[384,1536]{1,0:T(8,128)(2,1)S(1)}, bf16[384,1536]{1,0:T(8,128)(2,1)S(1)}, u32[]{:S(2)}, u32[]{:S(2)}) collective-permute-start(bf16[384,1536]{1,0:T(8,128)(2,1)S(1)} %collective-permute-done.8), channel_id=1, source_target_pairs={{0,2},{2,0},{4,6},{6,4},{1,3},{3,1},{5,7},{7,5}} | collective-permute-start | bytes 3538952 | tf_op jit(solution)/shard_map/ppermute | solution.py:27
  236.9 49.7 %collective-permute-start.22 = (bf16[384,1536]{1,0:T(8,128)(2,1)}, bf16[384,1536]{1,0:T(8,128)(2,1)}, u32[]{:S(2)}, u32[]{:S(2)}) collective-permute-start(bf16[384,1536]{1,0:T(8,128)(2,1)} %collective-permute-done.14), channel_id=1, source_target_pairs={{0,4},{4,0},{2,6},{6,2},{1,5},{5,1},{3,7},{7,3}} | collective-permute-start | bytes 3538952 | tf_op jit(solution)/shard_map/ppermute | solution.py:31
  238.7 50.0 %collective-permute-start.24 = (bf16[384,1536]{1,0:T(8,128)(2,1)S(1)}, bf16[384,1536]{1,0:T(8,128)(2,1)}, u32[]{:S(2)}, u32[]{:S(2)}) collective-permute-start(bf16[384,1536]{1,0:T(8,128)(2,1)S(1)} %collective-permute-done.20), channel_id=1, source_target_pairs={{0,2},{2,0},{4,6},{6,4},{1,3},{3,1},{5,7},{7,5}} | collective-permute-start | bytes 3538952 | tf_op jit(solution)/shard_map/ppermute | solution.py:27
  242.3 48.6 %collective-permute-start.21 = (bf16[384,1536]{1,0:T(8,128)(2,1)S(1)}, bf16[384,1536]{1,0:T(8,128)(2,1)S(1)}, u32[]{:S(2)}, u32[]{:S(2)}) collective-permute-start(bf16[384,1536]{1,0:T(8,128)(2,1)S(1)} %collective-permute-done.20), channel_id=1, source_target_pairs={{0,1},{1,0},{2,3},{3,2},{4,5},{5,4},{6,7},{7,6}} | collective-permute-start | bytes 3538952 | tf_op jit(solution)/shard_map/ppermute | solution.py:35
  261.9 32.5 %collective-permute-start.11 = (bf16[384,1536]{1,0:T(8,128)(2,1)S(1)}, bf16[384,1536]{1,0:T(8,128)(2,1)S(1)}, u32[]{:S(2)}, u32[]{:S(2)}) collective-permute-start(bf16[384,1536]{1,0:T(8,128)(2,1)S(1)} %collective-permute-done.10), channel_id=1, source_target_pairs={{0,1},{1,0},{2,3},{3,2},{4,5},{5,4},{6,7},{7,6}} | collective-permute-start | bytes 3538952 | tf_op jit(solution)/shard_map/ppermute | solution.py:35
  265.4 65.2 %collective-permute-start.13 = (bf16[384,1536]{1,0:T(8,128)(2,1)S(1)}, bf16[384,1536]{1,0:T(8,128)(2,1)}, u32[]{:S(2)}, u32[]{:S(2)}) collective-permute-start(bf16[384,1536]{1,0:T(8,128)(2,1)S(1)} %collective-permute-done.12), channel_id=1, source_target_pairs={{0,1},{1,0},{2,3},{3,2},{4,5},{5,4},{6,7},{7,6}} | collective-permute-start | bytes 3538952 | tf_op jit(solution)/shard_map/ppermute | solution.py:35
  286.6 39.3 %collective-permute-start.23 = (bf16[384,1536]{1,0:T(8,128)(2,1)}, bf16[384,1536]{1,0:T(8,128)(2,1)}, u32[]{:S(2)}, u32[]{:S(2)}) collective-permute-start(bf16[384,1536]{1,0:T(8,128)(2,1)} %collective-permute-done.22), channel_id=1, source_target_pairs={{0,1},{1,0},{2,3},{3,2},{4,5},{5,4},{6,7},{7,6}} | collective-permute-start | bytes 3538952 | tf_op jit(solution)/shard_map/ppermute | solution.py:35
  288.7 44.3 %collective-permute-start.25 = (bf16[384,1536]{1,0:T(8,128)(2,1)}, bf16[384,1536]{1,0:T(8,128)(2,1)}, u32[]{:S(2)}, u32[]{:S(2)}) collective-permute-start(bf16[384,1536]{1,0:T(8,128)(2,1)} %collective-permute-done.24), channel_id=1, source_target_pairs={{0,1},{1,0},{2,3},{3,2},{4,5},{5,4},{6,7},{7,6}} | collective-permute-start | bytes 3538952 | tf_op jit(solution)/shard_map/ppermute | solution.py:35
  726.2 795.4 %all-gather.12.cloned.1.call-start = ((), (), s32[]{:S(2)}) async-start(), calls=%async_computation.7 | async-start | bytes 14155776 | tf_op jit(solution)/shard_map/all_gather | solution.py:596
  892.6 121.4 %all-to-all-start.3 = ((bf16[8,512,768]{2,1,0:T(8,128)(2,1)}), bf16[8,512,768]{2,1,0:T(8,128)(2,1)}, u32[]{:S(2)}, u32[]{:S(2)}) async-start(bf16[8,512,768]{2,1,0:T(8,128)(2,1)} %get-tuple-element.228), calls=%async_computation.3 | async-start | bytes 12582912 | tf_op jit(solution)/shard_map/all_to_all | solution.py:640
  991.3 26.2 %collective-permute-start.37 = (f32[2,384,768]{2,1,0:T(8,128)}, f32[2,384,768]{2,1,0:T(8,128)S(1)}, u32[]{:S(2)}, u32[]{:S(2)}) collective-permute-start(f32[2,384,768]{2,1,0:T(8,128)} %get-tuple-element.184), channel_id=1, source_target_pairs={{0,1},{1,0},{2,3},{3,2},{4,5},{5,4},{6,7},{7,6}} | collective-permute-start | bytes 7077896 | tf_op jit(solution)/shard_map/ppermute | solution.py:35
  1014.0 77.8 %all-to-all-start.1 = ((bf16[8,512,768]{2,1,0:T(8,128)(2,1)}), bf16[8,512,768]{2,1,0:T(8,128)(2,1)}, u32[]{:S(2)}, u32[]{:S(2)}) async-start(bf16[8,512,768]{2,1,0:T(8,128)(2,1)} %get-tuple-element.224), calls=%async_computation.1 | async-start | bytes 12582912 | tf_op jit(solution)/shard_map/all_to_all | solution.py:640
  1017.5 525.5 %all-gather.14.cloned.1.call-start = ((), (), s32[]{:S(2)}) async-start(), calls=%async_computation.8 | async-start | bytes 14155776 | tf_op jit(solution)/shard_map/all_gather | solution.py:596
  1075.8 192.1 %collective-permute-start.41 = (f32[2,512,1536]{2,1,0:T(8,128)}, f32[2,512,1536]{2,1,0:T(8,128)}, u32[]{:S(2)}, u32[]{:S(2)}) collective-permute-start(f32[2,512,1536]{2,1,0:T(8,128)} %get-tuple-element.196), channel_id=1, source_target_pairs={{0,1},{1,0},{2,3},{3,2},{4,5},{5,4},{6,7},{7,6}} | collective-permute-start | bytes 18874376 | tf_op jit(solution)/shard_map/ppermute | solution.py:35
  1091.8 217.0 %all-to-all-start = ((bf16[8,512,768]{2,1,0:T(8,128)(2,1)}), bf16[8,512,768]{2,1,0:T(8,128)(2,1)}, u32[]{:S(2)}, u32[]{:S(2)}) async-start(bf16[8,512,768]{2,1,0:T(8,128)(2,1)} %get-tuple-element.222), calls=%async_computation | async-start | bytes 12582912 | tf_op jit(solution)/shard_map/all_to_all | solution.py:640
  1095.9 161.7 %collective-permute-start.62 = (f32[2,384,768]{2,1,0:T(8,128)}, f32[2,384,768]{2,1,0:T(8,128)S(1)}, u32[]{:S(2)}, u32[]{:S(2)}) collective-permute-start(f32[2,384,768]{2,1,0:T(8,128)} %get-tuple-element.181), channel_id=1, source_target_pairs={{0,4},{4,0},{2,6},{6,2},{1,5},{5,1},{3,7},{7,3}} | collective-permute-start | bytes 7077896 | tf_op jit(solution)/shard_map/ppermute | solution.py:31
  1097.9 162.0 %collective-permute-start.59 = (f32[2,384,768]{2,1,0:T(8,128)}, f32[2,384,768]{2,1,0:T(8,128)S(1)}, u32[]{:S(2)}, u32[]{:S(2)}) collective-permute-start(f32[2,384,768]{2,1,0:T(8,128)} %get-tuple-element.180), channel_id=1, source_target_pairs={{0,2},{2,0},{4,6},{6,4},{1,3},{3,1},{5,7},{7,5}} | collective-permute-start | bytes 7077896 | tf_op jit(solution)/shard_map/ppermute | solution.py:27
  1099.4 208.9 %collective-permute-start.61 = (f32[2,384,768]{2,1,0:T(8,128)}, f32[2,384,768]{2,1,0:T(8,128)}, u32[]{:S(2)}, u32[]{:S(2)}) collective-permute-start(f32[2,384,768]{2,1,0:T(8,128)} %get-tuple-element.189), channel_id=1, source_target_pairs={{0,4},{4,0},{2,6},{6,2},{1,5},{5,1},{3,7},{7,3}} | collective-permute-start | bytes 7077896 | tf_op jit(solution)/shard_map/ppermute | solution.py:31
  1099.9 208.4 %collective-permute-start.58 = (f32[2,384,768]{2,1,0:T(8,128)}, f32[2,384,768]{2,1,0:T(8,128)}, u32[]{:S(2)}, u32[]{:S(2)}) collective-permute-start(f32[2,384,768]{2,1,0:T(8,128)} %get-tuple-element.178), channel_id=1, source_target_pairs={{0,2},{2,0},{4,6},{6,4},{1,3},{3,1},{5,7},{7,5}} | collective-permute-start | bytes 7077896 | tf_op jit(solution)/shard_map/ppermute | solution.py:27
  1259.4 98.6 %collective-permute-start.63 = (f32[2,384,768]{2,1,0:T(8,128)}, f32[2,384,768]{2,1,0:T(8,128)}, u32[]{:S(2)}, u32[]{:S(2)}) collective-permute-start(f32[2,384,768]{2,1,0:T(8,128)} %add.350), channel_id=1, source_target_pairs={{0,2},{2,0},{4,6},{6,4},{1,3},{3,1},{5,7},{7,5}} | collective-permute-start | bytes 7077896 | tf_op jit(solution)/shard_map/ppermute | solution.py:27
  1261.5 97.3 %collective-permute-start.60 = (f32[2,384,768]{2,1,0:T(8,128)}, f32[2,384,768]{2,1,0:T(8,128)}, u32[]{:S(2)}, u32[]{:S(2)}) collective-permute-start(f32[2,384,768]{2,1,0:T(8,128)} %add.347), channel_id=1, source_target_pairs={{0,4},{4,0},{2,6},{6,2},{1,5},{5,1},{3,7},{7,3}} | collective-permute-start | bytes 7077896 | tf_op jit(solution)/shard_map/ppermute | solution.py:31
  1301.9 76.6 %collective-permute-start.42 = (f32[2,384,768]{2,1,0:T(8,128)}, f32[2,384,768]{2,1,0:T(8,128)S(1)}, u32[]{:S(2)}, u32[]{:S(2)}) collective-permute-start(f32[2,384,768]{2,1,0:T(8,128)} %get-tuple-element.198), channel_id=1, source_target_pairs={{0,1},{1,0},{2,3},{3,2},{4,5},{5,4},{6,7},{7,6}} | collective-permute-start | bytes 7077896 | tf_op jit(solution)/shard_map/ppermute | solution.py:35
  1308.3 70.4 %collective-permute-start.43 = (f32[2,384,768]{2,1,0:T(8,128)}, f32[2,384,768]{2,1,0:T(8,128)}, u32[]{:S(2)}, u32[]{:S(2)}) collective-permute-start(f32[2,384,768]{2,1,0:T(8,128)} %get-tuple-element.199), channel_id=1, source_target_pairs={{0,1},{1,0},{2,3},{3,2},{4,5},{5,4},{6,7},{7,6}} | collective-permute-start | bytes 7077896 | tf_op jit(solution)/shard_map/ppermute | solution.py:35
  1308.3 70.8 %collective-permute-start.44 = (f32[2,384,768]{2,1,0:T(8,128)}, f32[2,384,768]{2,1,0:T(8,128)}, u32[]{:S(2)}, u32[]{:S(2)}) collective-permute-start(f32[2,384,768]{2,1,0:T(8,128)} %get-tuple-element.200), channel_id=1, source_target_pairs={{0,1},{1,0},{2,3},{3,2},{4,5},{5,4},{6,7},{7,6}} | collective-permute-start | bytes 7077896 | tf_op jit(solution)/shard_map/ppermute | solution.py:35
  1308.8 129.2 %all-to-all-start.2 = ((bf16[8,512,768]{2,1,0:T(8,128)(2,1)}), bf16[8,512,768]{2,1,0:T(8,128)(2,1)}, u32[]{:S(2)}, u32[]{:S(2)}) async-start(bf16[8,512,768]{2,1,0:T(8,128)(2,1)} %get-tuple-element.226), calls=%async_computation.2 | async-start | bytes 12582912 | tf_op jit(solution)/shard_map/all_to_all | solution.py:640
  1358.9 29.9 %collective-permute-start.45 = (f32[2,384,768]{2,1,0:T(8,128)}, f32[2,384,768]{2,1,0:T(8,128)}, u32[]{:S(2)}, u32[]{:S(2)}) collective-permute-start(f32[2,384,768]{2,1,0:T(8,128)} %get-tuple-element.201), channel_id=1, source_target_pairs={{0,1},{1,0},{2,3},{3,2},{4,5},{5,4},{6,7},{7,6}} | collective-permute-start | bytes 7077896 | tf_op jit(solution)/shard_map/ppermute | solution.py:35
  1378.1 35.0 %collective-permute-start.46 = (f32[2,384,768]{2,1,0:T(8,128)}, f32[2,384,768]{2,1,0:T(8,128)}, u32[]{:S(2)}, u32[]{:S(2)}) collective-permute-start(f32[2,384,768]{2,1,0:T(8,128)} %get-tuple-element.208), channel_id=1, source_target_pairs={{0,1},{1,0},{2,3},{3,2},{4,5},{5,4},{6,7},{7,6}} | collective-permute-start | bytes 7077896 | tf_op jit(solution)/shard_map/ppermute | solution.py:35
  1378.5 35.0 %collective-permute-start.47 = (f32[2,384,768]{2,1,0:T(8,128)}, f32[2,384,768]{2,1,0:T(8,128)}, u32[]{:S(2)}, u32[]{:S(2)}) collective-permute-start(f32[2,384,768]{2,1,0:T(8,128)} %get-tuple-element.209), channel_id=1, source_target_pairs={{0,1},{1,0},{2,3},{3,2},{4,5},{5,4},{6,7},{7,6}} | collective-permute-start | bytes 7077896 | tf_op jit(solution)/shard_map/ppermute | solution.py:35
  1378.7 35.0 %collective-permute-start.48 = (f32[2,384,768]{2,1,0:T(8,128)}, f32[2,384,768]{2,1,0:T(8,128)}, u32[]{:S(2)}, u32[]{:S(2)}) collective-permute-start(f32[2,384,768]{2,1,0:T(8,128)} %get-tuple-element.210), channel_id=1, source_target_pairs={{0,1},{1,0},{2,3},{3,2},{4,5},{5,4},{6,7},{7,6}} | collective-permute-start | bytes 7077896 | tf_op jit(solution)/shard_map/ppermute | solution.py:35
  1379.1 37.1 %collective-permute-start.49 = (f32[2,384,768]{2,1,0:T(8,128)}, f32[2,384,768]{2,1,0:T(8,128)}, u32[]{:S(2)}, u32[]{:S(2)}) collective-permute-start(f32[2,384,768]{2,1,0:T(8,128)} %get-tuple-element.211), channel_id=1, source_target_pairs={{0,1},{1,0},{2,3},{3,2},{4,5},{5,4},{6,7},{7,6}} | collective-permute-start | bytes 7077896 | tf_op jit(solution)/shard_map/ppermute | solution.py:35
  1388.7 75.7 %collective-permute-start.66 = (bf16[2048,1536]{1,0:T(8,128)(2,1)}, bf16[2048,1536]{1,0:T(8,128)(2,1)}, u32[]{:S(2)}, u32[]{:S(2)}) collective-permute-start(bf16[2048,1536]{1,0:T(8,128)(2,1)} %bitcast.28), channel_id=1, source_target_pairs={{0,1},{1,0},{2,3},{3,2},{4,5},{5,4},{6,7},{7,6}} | collective-permute-start | bytes 18874376 | tf_op jit(solution)/shard_map/ppermute | solution.py:35
  1413.1 125.0 %collective-permute-start.65 = (f32[768,768]{1,0:T(8,128)}, f32[768,768]{1,0:T(8,128)}, u32[]{:S(2)}, u32[]{:S(2)}) collective-permute-start(f32[768,768]{1,0:T(8,128)} %bitcast.26.ob_ref), channel_id=1, source_target_pairs={{0,1},{1,0},{2,3},{3,2},{4,5},{5,4},{6,7},{7,6}} | collective-permute-start | bytes 7077896 | tf_op jit(solution)/shard_map/ppermute | solution.py:35
  1413.6 128.5 %collective-permute-start.64 = (f32[768,768]{1,0:T(8,128)}, f32[768,768]{1,0:T(8,128)}, u32[]{:S(2)}, u32[]{:S(2)}) collective-permute-start(f32[768,768]{1,0:T(8,128)} %bitcast.25.oa_ref), channel_id=1, source_target_pairs={{0,1},{1,0},{2,3},{3,2},{4,5},{5,4},{6,7},{7,6}} | collective-permute-start | bytes 7077896 | tf_op jit(solution)/shard_map/ppermute | solution.py:35
  1413.6 61.9 %collective-permute-start.71 = (bf16[512,1536]{1,0:T(8,128)(2,1)S(1)}, bf16[512,1536]{1,0:T(8,128)(2,1)}, u32[]{:S(2)}, u32[]{:S(2)}) collective-permute-start(bf16[512,1536]{1,0:T(8,128)(2,1)S(1)} %get-tuple-element.247), channel_id=1, source_target_pairs={{0,2},{2,0},{5,7},{7,5}} | collective-permute-start | bytes 4718600 | tf_op jit(solution)/shard_map/ppermute | solution.py:682
  1416.1 68.0 %collective-permute-start.54 = (f32[2,384,768]{2,1,0:T(8,128)}, f32[2,384,768]{2,1,0:T(8,128)}, u32[]{:S(2)}, u32[]{:S(2)}) collective-permute-start(f32[2,384,768]{2,1,0:T(8,128)} %get-tuple-element.203), channel_id=1, source_target_pairs={{0,4},{4,0},{2,6},{6,2},{1,5},{5,1},{3,7},{7,3}} | collective-permute-start | bytes 7077896 | tf_op jit(solution)/shard_map/ppermute | solution.py:31
  1464.5 53.9 %collective-permute-start.51 = (f32[2,384,768]{2,1,0:T(8,128)S(1)}, f32[2,384,768]{2,1,0:T(8,128)S(1)}, u32[]{:S(2)}, u32[]{:S(2)}) collective-permute-start(f32[2,384,768]{2,1,0:T(8,128)S(1)} %copy-done.31), channel_id=1, source_target_pairs={{0,2},{2,0},{4,6},{6,4},{1,3},{3,1},{5,7},{7,5}} | collective-permute-start | bytes 7077896 | tf_op jit(solution)/shard_map/ppermute | solution.py:27
  1475.6 67.4 %collective-permute-start.69 = (bf16[512,1536]{1,0:T(8,128)(2,1)}, bf16[512,1536]{1,0:T(8,128)(2,1)}, u32[]{:S(2)}, u32[]{:S(2)}) collective-permute-start(bf16[512,1536]{1,0:T(8,128)(2,1)} %get-tuple-element.246), channel_id=1, source_target_pairs={{0,4},{2,6},{5,1},{7,3}} | collective-permute-start | bytes 4718600 | tf_op jit(solution)/shard_map/ppermute | solution.py:681
  1484.1 80.5 %collective-permute-start.53 = (f32[2,384,768]{2,1,0:T(8,128)}, f32[2,384,768]{2,1,0:T(8,128)}, u32[]{:S(2)}, u32[]{:S(2)}) collective-permute-start(f32[2,384,768]{2,1,0:T(8,128)} %get-tuple-element.215), channel_id=1, source_target_pairs={{0,4},{4,0},{2,6},{6,2},{1,5},{5,1},{3,7},{7,3}} | collective-permute-start | bytes 7077896 | tf_op jit(solution)/shard_map/ppermute | solution.py:31
  1518.3 118.0 %collective-permute-start.50 = (f32[2,384,768]{2,1,0:T(8,128)}, f32[2,384,768]{2,1,0:T(8,128)}, u32[]{:S(2)}, u32[]{:S(2)}) collective-permute-start(f32[2,384,768]{2,1,0:T(8,128)} %get-tuple-element.204), channel_id=1, source_target_pairs={{0,2},{2,0},{4,6},{6,4},{1,3},{3,1},{5,7},{7,5}} | collective-permute-start | bytes 7077896 | tf_op jit(solution)/shard_map/ppermute | solution.py:27
  1538.1 122.3 %collective-permute-start.72 = (bf16[1024,1536]{1,0:T(8,128)(2,1)}, bf16[1024,1536]{1,0:T(8,128)(2,1)}, u32[]{:S(2)}, u32[]{:S(2)}) collective-permute-start(bf16[1024,1536]{1,0:T(8,128)(2,1)} %pad_maximum_fusion.3), channel_id=1, source_target_pairs={{0,4},{2,6},{5,1},{7,3}} | collective-permute-start | bytes 9437192 | tf_op jit(solution)/shard_map/ppermute | solution.py:686
  1542.1 80.2 %collective-permute-start.55 = (f32[2,384,768]{2,1,0:T(8,128)}, f32[2,384,768]{2,1,0:T(8,128)}, u32[]{:S(2)}, u32[]{:S(2)}) collective-permute-start(f32[2,384,768]{2,1,0:T(8,128)} %add.344), channel_id=1, source_target_pairs={{0,2},{2,0},{4,6},{6,4},{1,3},{3,1},{5,7},{7,5}} | collective-permute-start | bytes 7077896 | tf_op jit(solution)/shard_map/ppermute | solution.py:27
  1543.0 93.4 %collective-permute-start.52 = (f32[2,384,768]{2,1,0:T(8,128)}, f32[2,384,768]{2,1,0:T(8,128)}, u32[]{:S(2)}, u32[]{:S(2)}) collective-permute-start(f32[2,384,768]{2,1,0:T(8,128)} %add.341), channel_id=1, source_target_pairs={{0,4},{4,0},{2,6},{6,2},{1,5},{5,1},{3,7},{7,3}} | collective-permute-start | bytes 7077896 | tf_op jit(solution)/shard_map/ppermute | solution.py:31
  1564.6 109.8 %collective-permute-start.67 = (f32[768,1536]{1,0:T(8,128)}, f32[768,1536]{1,0:T(8,128)}, u32[]{:S(2)}, u32[]{:S(2)}) collective-permute-start(f32[768,1536]{1,0:T(8,128)} %add_add_fusion.refs_0_), channel_id=1, source_target_pairs={{0,1},{1,0},{2,3},{3,2},{4,5},{5,4},{6,7},{7,6}} | collective-permute-start | bytes 14155784 | tf_op jit(solution)/shard_map/ppermute | solution.py:35
  1622.3 36.0 %collective-permute-start.70 = (bf16[512,1536]{1,0:T(8,128)(2,1)}, bf16[512,1536]{1,0:T(8,128)(2,1)}, u32[]{:S(2)}, u32[]{:S(2)}) collective-permute-start(bf16[512,1536]{1,0:T(8,128)(2,1)} %broadcast_select_fusion.3), channel_id=1, source_target_pairs={{0,2},{2,0},{4,6},{6,4},{1,3},{3,1},{5,7},{7,5}} | collective-permute-start | bytes 4718600 | tf_op jit(solution)/shard_map/ppermute | solution.py:27
  1636.4 28.1 %collective-permute-start.57 = (f32[2,384,768]{2,1,0:T(8,128)S(1)}, f32[2,384,768]{2,1,0:T(8,128)S(1)}, u32[]{:S(2)}, u32[]{:S(2)}) collective-permute-start(f32[2,384,768]{2,1,0:T(8,128)S(1)} %add_add_fusion.3.own_b), channel_id=1, source_target_pairs={{0,1},{1,0},{2,3},{3,2},{4,5},{5,4},{6,7},{7,6}} | collective-permute-start | bytes 7077896 | tf_op jit(solution)/shard_map/ppermute | solution.py:35
  (54 other events, 2196.3 us)
Sparse Core Ops, SparseCore 0:
  16.2 129.7 all-gather.5
  148.4 52.1 all-gather.7
  726.3 66.6 all-gather.9
  821.8 66.5 all-gather.11
  1076.3 149.7 all-gather.13

commit v10 on v9

--- a/solution.py
+++ b/solution.py
@@ -67,8 +67,8 @@
 
 
 def attn_fwd_body(*refs):
-    q_ref, qn_ref, ko_ref, ks_ref, kno_ref, kns_ref, vo_ref, vs_ref = refs[:8]
-    ctx_ref, lse_ref, a_ref, ma_ref = refs[-4:]
+    u_ref, w0_ref, wn_ref, ko_ref, ks_ref, kno_ref, kns_ref, vo_ref, vs_ref = refs[:9]
+    q_ref, ctx_ref, lse_ref, qs_ref, a_ref, ma_ref = refs[-6:]
     units = [(sub, i) for sub in range(WIDE // 128) for i in range(q_ref.shape[0] // CHUNK)]
 
     def joined(own_ref, sib_ref, sub):
@@ -81,14 +81,18 @@
 
     @pl.when(pl.program_id(0) == 0)
     def _():
-        a_ref[...], ma_ref[...] = scores(ko_ref, ks_ref, q_ref, 0, 0)
-
+        qs_ref[...] = nt(u_ref[0, 0], w0_ref[...]).astype(BF16)
+        a_ref[...], ma_ref[...] = scores(ko_ref, ks_ref, qs_ref[...], 0, 0)
+
+    q_ref[...] = qs_ref[...]
     s, m = a_ref[...], ma_ref[...]
     for n, (sub, i) in enumerate(units):
         if n + 1 < len(units):
-            ahead = scores(ko_ref, ks_ref, q_ref, *units[n + 1])
+            ahead = scores(ko_ref, ks_ref, q_ref[...], *units[n + 1])
         else:
-            ahead = scores(kno_ref, kns_ref, qn_ref, 0, 0)
+            ahead = scores(kno_ref, kns_ref, q_next, 0, 0)
+        if n == 0:
+            q_next = nt(u_ref[0, 0], wn_ref[...]).astype(BF16)
         rows, cols = slice(i * CHUNK, (i + 1) * CHUNK), slice(sub * 128, (sub + 1) * 128)
         p = jnp.exp2((s - m) * (SCALE * LOG2E))
         l = jnp.sum(p, axis=0, keepdims=True)
@@ -100,12 +104,13 @@
         ctx_t = jnp.concatenate([ctx_t[:HEAD_DIM, :CHUNK], ctx_t[HEAD_DIM:, CHUNK:]], axis=0)
         ctx_ref[0, 0, rows, cols] = ctx_t.T.astype(BF16)
         s, m = ahead
+    qs_ref[...] = q_next
     a_ref[...], ma_ref[...] = s, m
 
 
-def attn_fwd(q, kv, kv_s, layer, layers, hist):
-    tq, width = q.shape
-    tk = kv.shape[0]
+def attn_fwd(um_hist, wq, kv, kv_s, layer, layers, hist):
+    tk, width = kv.shape[0], kv.shape[1] // 2
+    tq = um_hist.shape[2]
     pairs = width // 128
     steps = width // WIDE
 
@@ -120,23 +125,27 @@
     return pl.pallas_call(
         attn_fwd_body,
         grid=(steps,),
-        in_specs=[pl.BlockSpec((tq, WIDE), col(0)), pl.BlockSpec((tq, WIDE), nxt),
+        in_specs=[pl.BlockSpec((1, 1, tq, width), lambda j: (0, layer, 0, 0)),
+                  pl.BlockSpec((WIDE, width), lambda j: (0, 0)),
+                  pl.BlockSpec((WIDE, width), lambda j: (jnp.minimum(j + 1, steps - 1), 0)),
                   pl.BlockSpec((tk, WIDE), col(0)), pl.BlockSpec((tk, WIDE), col(0)),
                   pl.BlockSpec((tk, WIDE), nxt), pl.BlockSpec((tk, WIDE), nxt),
                   pl.BlockSpec((tk, WIDE), col(steps)), pl.BlockSpec((tk, WIDE), col(steps))]
         + [pl.BlockSpec(memory_space=pl.ANY)] * len(extra),
-        out_specs=[pl.BlockSpec((1, 1, tq, WIDE), lambda j: (3, layer, 0, j)),
+        out_specs=[pl.BlockSpec((tq, WIDE), col(0)),
+                   pl.BlockSpec((1, 1, tq, WIDE), lambda j: (3, layer, 0, j)),
                    pl.BlockSpec((WIDE // 128, 2, tq), lambda j: (j, 0, 0))],
-        out_shape=[jax.ShapeDtypeStruct((4, layers, tq, width), BF16),
+        out_shape=[jax.ShapeDtypeStruct((tq, width), BF16),
+                   jax.ShapeDtypeStruct((4, layers, tq, width), BF16),
                    jax.ShapeDtypeStruct((pairs, 2, tq), F32)],
-        input_output_aliases={8: 0} if extra else {},
-        scratch_shapes=[pltpu.VMEM((2 * tk, 2 * CHUNK), F32), pltpu.VMEM((1, 2 * CHUNK), F32)],
+        input_output_aliases={9: 1} if extra else {},
+        scratch_shapes=[pltpu.VMEM((tq, WIDE), BF16), pltpu.VMEM((2 * tk, 2 * CHUNK), F32), pltpu.VMEM((1, 2 * CHUNK), F32)],
         compiler_params=pltpu.CompilerParams(dimension_semantics=('arbitrary',),
                                              vmem_limit_bytes=VMEM_ALL),
         cost_estimate=pl.CostEstimate(flops=flops, bytes_accessed=2 * (tq * width * 2 + 4 * tk * width),
                                       transcendentals=tq * 2 * tk * (width // HEAD_DIM)),
         name='attn_fwd',
-    )(q, q, kv, kv_s, kv, kv_s, kv, kv_s, *extra)
+    )(um_hist, wq, wq, kv, kv_s, kv, kv_s, kv, kv_s, *extra)
 
 
 def attn_bwd_body(q_ref, ko_ref, ks_ref, vo_ref, vs_ref, do_ref, lse_ref, hist_ref, dq_ref, down_ref, dsib_ref):
@@ -485,6 +494,32 @@
     )(d_next, h, z, wo, w1t, w2, *extra)
 
 
+def spread_body(chips_ref, src_ref, q_ref, kv_ref):
+    @pl.when(pl.program_id(0) < 4)
+    def _():
+        q_ref[...] = src_ref[...]
+
+    @pl.when(pl.program_id(0) >= 4)
+    def _():
+        kv_ref[...] = src_ref[...]
+
+
+def spread(chips, qkv):
+    rows, dim = qkv.shape[0] // 12, qkv.shape[1]
+    return pl.pallas_call(
+        spread_body,
+        grid_spec=pltpu.PrefetchScalarGridSpec(
+            num_scalar_prefetch=1, grid=(12,),
+            in_specs=[pl.BlockSpec((rows, dim), lambda i, c: (3 * c[i % 4] + i // 4, 0))],
+            out_specs=[pl.BlockSpec((rows, dim), lambda i, c: (jnp.minimum(i, 3), 0)),
+                       pl.BlockSpec((rows, dim), lambda i, c: (jnp.maximum(i - 4, 0), 0))]),
+        out_shape=[jax.ShapeDtypeStruct((4 * rows, dim), BF16), jax.ShapeDtypeStruct((8 * rows, dim), BF16)],
+        compiler_params=pltpu.CompilerParams(dimension_semantics=('arbitrary',), vmem_limit_bytes=VMEM_ALL),
+        cost_estimate=pl.CostEstimate(flops=qkv.size, bytes_accessed=4 * qkv.size, transcendentals=0),
+        name='spread',
+    )(chips, qkv)
+
+
 def join_body(count, core_ref, *refs):
     for n in range(count):
         own, other, out = refs[n], refs[count + n], refs[2 * count + n]
@@ -621,8 +656,7 @@
         o_all = gather(take(w_o, core, 0, hid // 2))
         w2 = gather_permuted(w_2)
         w1 = gather_permuted(w_1.T)
-        wq = jnp.concatenate([take(qkv_all, 3 * c, 0, hid) for c in chips], axis=0)
-        wkv = jnp.concatenate([take(qkv_all, 3 * c + i, 0, hid) for i in (1, 2) for c in chips], axis=0)
+        wq, wkv = spread(jnp.stack(chips).astype(jnp.int32), qkv_all)
         wo = jnp.concatenate([take(o_all, c, 0, hid) for c in chips], axis=0)
         d_cur = my_tokens(cot_out)
         emb = step_emb.astype(F32)
@@ -634,8 +668,7 @@
             e = emb[layer:layer + 1]
             kv, um_hist = norm_kv(x_cur, e, wkv, layer, layer_count, um_hist)
             kv_s = pp_d(kv)
-            q = nt(um_hist[0, layer], wq).astype(BF16)
-            att_hist, lse = attn_fwd(q, kv, kv_s, layer, layer_count, att_hist)
+            q, att_hist, lse = attn_fwd(um_hist, wq, kv, kv_s, layer, layer_count, att_hist)
             z, g, x_next, h, m_hist = mlp_fwd(x_cur, e, att_hist, wo, w1, w2, layer, layer_count, m_hist)
             g_mine.append(lax.all_to_all(g.reshape(-1, g.shape[-1]), BOTH, split_axis=0, concat_axis=0, tiled=True))
             saved.append((x_cur, q, kv, kv_s, lse, h, z))

time: 1700 us -> 1720 us (1.012)
  Pallas kernels: 791 us -> 819 us
  waiting for transfers between devices: 539 us -> 564 us
  matrix products: 125 us -> 101 us
  local copies, waits for them, and re-layouts: 109 us -> 91.4 us
    pallas_call x4 -> x5, Pallas kernels: 86.8 us -> 114 us  [the longest x4 99.5 us: attn_fwd(): pl.pallas_call(attn_fwd_body, grid=(steps,), in_specs=[pl.BlockSpec((1, 1...]
    dot_general x13 -> x9, matrix products: 125 us -> 101 us  [dot(): return lax.dot_general(a, b, (dims, ((), ())), preferred_element_type=F32)]
    ppermute x12, waiting for transfers between devices: 223 us -> 241 us  [pp_y(): return lax.ppermute(v, 'model', SWAP_Y)]
    unnamed x83 -> x54, local copies, waits for them, and re-layouts: 33.9 us -> 16.6 us
  transfers between devices with their start and end apart: 82 -> 82, of which waited for: 23 -> 22; matrix products, arithmetic and copies ran while one was open for 16% -> 14% of each run, Pallas kernels for 26% -> 27%
where the time goes in v10:
time: 1720 us; the launch traced here: 1710 us
  Pallas kernels  819 us (48%)
  waiting for transfers between devices  564 us (33%)
  matrix products  101 us (6%)
  local copies, waits for them, and re-layouts  91.4 us (5%)
  starting transfers between devices  63.1 us (4%)
  other arithmetic  55 us (3%)
    ppermute x13, waiting for transfers between devices, pp_x(): return lax.ppermute(v, 'model', SWAP_X)  283 us
    ppermute x12, waiting for transfers between devices, pp_y(): return lax.ppermute(v, 'model', SWAP_Y)  241 us
    pallas_call x8, Pallas kernels, terms(): pl.pallas_call(functools.partial(terms_body, len(recv) // 4, slot_of), gr...  163 us
    pallas_call x4, Pallas kernels, attn_bwd(): pl.pallas_call(attn_bwd_body, grid=(steps,), in_specs=[qblk, kblk, kblk,...  144 us
    pallas_call x4, Pallas kernels, mlp_bwd(): pl.pallas_call(mlp_bwd_body, grid=(hidden // BLOCK_B,), in_specs=[whole,...  138 us
    pallas_call x4, Pallas kernels, mlp_fwd(): pl.pallas_call(mlp_fwd_body, grid=(hidden // BLOCK_F,), in_specs=[whole,...  135 us
    dot_general x9, matrix products, dot(): return lax.dot_general(a, b, (dims, ((), ())), preferred_element_type=F32)  101 us
    pallas_call x4, Pallas kernels, attn_fwd(): pl.pallas_call(attn_fwd_body, grid=(steps,), in_specs=[pl.BlockSpec((1, 1...  99.5 us
  transfers between devices with their start and end apart: 82, of which 22 were waited for; matrix products, arithmetic and copies ran while one was open for 14% of the time, Pallas kernels for 27%

profile of v10, /device:TPU:0, one launch (start us, length us, event | category | flops | bytes accessed | tf_op | source)
XLA Modules:
  0.0 1708.2 jit_solution(3892585986999407613)
XLA Ops:
  16.2 6.6 copy.43
  40.5 7.3 broadcast.6.clone
  51.5 25.1 %collective-permute-done.2 = bf16[384,1536]{1,0:T(8,128)(2,1)} collective-permute-done((bf16[384,1536]{1,0:T(8,128)(2,1)}, bf16[384,1536]{1,0:T(8,128)(2,1)}, u32[]{:S(2)}, u32[]{:S(2)}) %collective-permute-start.2) | collective-permute-done | bytes 1179680 | tf_op jit(solution)/shard_map/ppermute | solution.py:27
  77.1 6.5 broadcast.6.clone.1
  86.0 41.1 %collective-permute-done.4 = bf16[384,1536]{1,0:T(8,128)(2,1)} collective-permute-done((bf16[384,1536]{1,0:T(8,128)(2,1)}, bf16[384,1536]{1,0:T(8,128)(2,1)}, u32[]{:S(2)}, u32[]{:S(2)}) %collective-permute-start.4) | collective-permute-done | bytes 1179680 | tf_op jit(solution)/shard_map/ppermute | solution.py:27
  130.2 35.9 %collective-permute-done.14 = bf16[384,1536]{1,0:T(8,128)(2,1)} collective-permute-done((bf16[384,1536]{1,0:T(8,128)(2,1)}, bf16[384,1536]{1,0:T(8,128)(2,1)}, u32[]{:S(2)}, u32[]{:S(2)}) %collective-permute-start.14) | collective-permute-done | bytes 1179680 | tf_op jit(solution)/shard_map/ppermute | solution.py:27
  175.7 29.5 %collective-permute-done.16 = bf16[384,1536]{1,0:T(8,128)(2,1)S(1)} collective-permute-done((bf16[384,1536]{1,0:T(8,128)(2,1)S(1)}, bf16[384,1536]{1,0:T(8,128)(2,1)S(1)}, u32[]{:S(2)}, u32[]{:S(2)}) %collective-permute-start.16) | collective-permute-done | bytes 1179680 | tf_op jit(solution)/shard_map/ppermute | solution.py:27
  215.6 17.5 %collective-permute-done.8 = bf16[384,1536]{1,0:T(8,128)(2,1)S(1)} collective-permute-done((bf16[384,1536]{1,0:T(8,128)(2,1)}, bf16[384,1536]{1,0:T(8,128)(2,1)S(1)}, u32[]{:S(2)}, u32[]{:S(2)}) %collective-permute-start.8) | collective-permute-done | bytes 1179680 | tf_op jit(solution)/shard_map/ppermute | solution.py:31
  235.8 22.5 %collective-permute-done.20 = bf16[384,1536]{1,0:T(8,128)(2,1)S(1)} collective-permute-done((bf16[384,1536]{1,0:T(8,128)(2,1)S(1)}, bf16[384,1536]{1,0:T(8,128)(2,1)S(1)}, u32[]{:S(2)}, u32[]{:S(2)}) %collective-permute-start.20) | collective-permute-done | bytes 1179680 | tf_op jit(solution)/shard_map/ppermute | solution.py:31
  267.5 16.2 collective-permute-done.10
  287.2 21.2 %collective-permute-done.22 = bf16[384,1536]{1,0:T(8,128)(2,1)S(1)} collective-permute-done((bf16[384,1536]{1,0:T(8,128)(2,1)}, bf16[384,1536]{1,0:T(8,128)(2,1)S(1)}, u32[]{:S(2)}, u32[]{:S(2)}) %collective-permute-start.22) | collective-permute-done | bytes 1179680 | tf_op jit(solution)/shard_map/ppermute | solution.py:31
  311.8 14.7 spread.1
  326.5 9.9 norm_kv.4
  357.1 24.9 %attn_fwd.4 = (bf16[512,1536]{1,0:T(8,128)(2,1)}, bf16[4,4,512,1536]{3,2,1,0:T(8,128)(2,1)}, f32[12,2,512]{2,1,0:T(2,128)}) custom-call(bf16[2,4,512,1536]{3,2,1,0:T(8,128)(2,1)} %get-tuple-element.126.refs_0_.refs_3_, bf16[1536,1536]{1,0:T(8,128)(2,1)} %get-tuple-element.127.refs_1_.refs_2_, bf16[1536,1536]{1,0:T(8,128)(2,1)} %get-tuple-element.127.refs_1_.refs_2_, ...), custom_call_target="tpu_custom_call" | custom-call | flops 12884901888 | bytes 9437184 | tf_op jit(solution)/shard_map/attn_fwd/pallas_call | solution.py:125
  382.0 33.7 %mlp_fwd.4 = (bf16[512,6144]{1,0:T(8,128)(2,1)}, bf16[8,512,768]{2,1,0:T(8,128)(2,1)}, bf16[512,1536]{1,0:T(8,128)(2,1)}, bf16[512,1536]{1,0:T(8,128)(2,1)}, bf16[4,512,1536]{2,1,0:T(8,128)(2,1)}) custom-call(bf16[512,1536]{1,0:T(8,128)(2,1)} %bitcast_select_fusion.1.refs_0_.x_hbm, f32[1,1536]{1,0:T(1,128)} %get-tuple-element.262.refs_1_.e_ref, ...), custom_call_target="tpu_custom_call" | custom-call | flops 19327352832 | bytes 50331648 | tf_op jit(solution)/shard_map/mlp_fwd/pallas_call | solution.py:409
  415.7 10.0 norm_kv.5
  426.2 5.6 collective-permute-done.26.refs_4_.refs_6_.refs_8_.ks_ref.vs_ref
  431.9 24.8 %attn_fwd.5 = (bf16[512,1536]{1,0:T(8,128)(2,1)}, bf16[4,4,512,1536]{3,2,1,0:T(8,128)(2,1)}, f32[12,2,512]{2,1,0:T(2,128)}) custom-call(bf16[2,4,512,1536]{3,2,1,0:T(8,128)(2,1)} %get-tuple-element.132.refs_0_.refs_3_, bf16[1536,1536]{1,0:T(8,128)(2,1)} %get-tuple-element.127.refs_1_.refs_2_, ...), custom_call_target="tpu_custom_call", output_to_operand_aliasing={{1}: (9, {})} | custom-call | flops 12884901888 | bytes 9437184 | tf_op jit(solution)/shard_map/attn_fwd/pallas_call | solution.py:125
  456.7 33.8 %mlp_fwd.5 = (bf16[512,6144]{1,0:T(8,128)(2,1)}, bf16[8,512,768]{2,1,0:T(8,128)(2,1)}, bf16[512,1536]{1,0:T(8,128)(2,1)}, bf16[512,1536]{1,0:T(8,128)(2,1)}, bf16[4,512,1536]{2,1,0:T(8,128)(2,1)}) custom-call(bf16[512,1536]{1,0:T(8,128)(2,1)} %get-tuple-element.131.refs_0_.x_hbm, ...), custom_call_target="tpu_custom_call", output_to_operand_aliasing={{4}: (6, {})} | custom-call | flops 19327352832 | bytes 50331648 | tf_op jit(solution)/shard_map/mlp_fwd/pallas_call | solution.py:409
  490.5 9.9 norm_kv.6
  500.8 5.6 collective-permute-done.27.refs_4_.refs_6_.refs_8_.ks_ref.vs_ref
  506.4 24.9 %attn_fwd.6 = (bf16[512,1536]{1,0:T(8,128)(2,1)}, bf16[4,4,512,1536]{3,2,1,0:T(8,128)(2,1)}, f32[12,2,512]{2,1,0:T(2,128)}) custom-call(bf16[2,4,512,1536]{3,2,1,0:T(8,128)(2,1)} %get-tuple-element.138.refs_0_.refs_3_, bf16[1536,1536]{1,0:T(8,128)(2,1)} %get-tuple-element.127.refs_1_.refs_2_, ...), custom_call_target="tpu_custom_call", output_to_operand_aliasing={{1}: (9, {})} | custom-call | flops 12884901888 | bytes 9437184 | tf_op jit(solution)/shard_map/attn_fwd/pallas_call | solution.py:125
  531.3 34.0 %mlp_fwd.6 = (bf16[512,6144]{1,0:T(8,128)(2,1)}, bf16[8,512,768]{2,1,0:T(8,128)(2,1)}, bf16[512,1536]{1,0:T(8,128)(2,1)}, bf16[512,1536]{1,0:T(8,128)(2,1)}, bf16[4,512,1536]{2,1,0:T(8,128)(2,1)}) custom-call(bf16[512,1536]{1,0:T(8,128)(2,1)} %get-tuple-element.137.refs_0_.x_hbm, ...), custom_call_target="tpu_custom_call", output_to_operand_aliasing={{4}: (6, {})} | custom-call | flops 19327352832 | bytes 50331648 | tf_op jit(solution)/shard_map/mlp_fwd/pallas_call | solution.py:409
  565.2 10.0 norm_kv.7
  577.5 5.8 collective-permute-done.29
  586.5 24.9 %attn_fwd.7 = (bf16[512,1536]{1,0:T(8,128)(2,1)}, bf16[4,4,512,1536]{3,2,1,0:T(8,128)(2,1)}, f32[12,2,512]{2,1,0:T(2,128)}) custom-call(bf16[2,4,512,1536]{3,2,1,0:T(8,128)(2,1)} %get-tuple-element.144.refs_0_.refs_6_, bf16[1536,1536]{1,0:T(8,128)(2,1)} %get-tuple-element.127.refs_1_.refs_2_, ...), custom_call_target="tpu_custom_call", output_to_operand_aliasing={{1}: (9, {})} | custom-call | flops 12884901888 | bytes 9437184 | tf_op jit(solution)/shard_map/attn_fwd/pallas_call | solution.py:125
  611.4 33.7 %mlp_fwd.7 = (bf16[512,6144]{1,0:T(8,128)(2,1)}, bf16[8,512,768]{2,1,0:T(8,128)(2,1)}, bf16[512,1536]{1,0:T(8,128)(2,1)}, bf16[512,1536]{1,0:T(8,128)(2,1)}, bf16[4,512,1536]{2,1,0:T(8,128)(2,1)}) custom-call(bf16[512,1536]{1,0:T(8,128)(2,1)} %get-tuple-element.143.refs_0_.x_hbm, ...), custom_call_target="tpu_custom_call", output_to_operand_aliasing={{4}: (6, {})} | custom-call | flops 19327352832 | bytes 50331648 | tf_op jit(solution)/shard_map/mlp_fwd/pallas_call | solution.py:409
  645.1 34.0 %mlp_bwd.4 = (bf16[4,512,6144]{2,1,0:T(8,128)(2,1)}, bf16[2,4,512,1536]{3,2,1,0:T(8,128)(2,1)}, bf16[512,1536]{1,0:T(8,128)(2,1)}) custom-call(bf16[512,1536]{1,0:T(8,128)(2,1)} %bitcast_select_fusion.refs_0_, bf16[512,1536]{1,0:T(8,128)(2,1)} %get-tuple-element.149.refs_1_, ...), custom_call_target="tpu_custom_call", output_to_operand_aliasing={{1}: (6, {})} | custom-call | flops 19327352832 | bytes 50331648 | tf_op jit(solution)/shard_map/mlp_bwd/pallas_call | solution.py:479
  679.1 36.0 %attn_bwd.4 = (bf16[4,4,512,1536]{3,2,1,0:T(8,128)(2,1)}, f32[2,512,1536]{2,1,0:T(8,128)}, f32[2,512,1536]{2,1,0:T(8,128)}) custom-call(bf16[512,1536]{1,0:T(8,128)(2,1)} %get-tuple-element.146.q_ref, bf16[512,3072]{1,0:T(8,128)(2,1)} %get-tuple-element.145.refs_3_.refs_5_.refs_7_.ko_ref.vo_ref, ...), custom_call_target="tpu_custom_call", output_to_operand_aliasing={{0}: (7, {})} | custom-call | flops 32212254720 | bytes 25165824 | tf_op jit(solution)/shard_map/attn_bwd/pallas_call | solution.py:206
  715.5 7.1 fusion.13.acc0_hbm
  725.7 14.5 d_kv.4
  740.2 35.2 %mlp_bwd.5 = (bf16[4,512,6144]{2,1,0:T(8,128)(2,1)}, bf16[2,4,512,1536]{3,2,1,0:T(8,128)(2,1)}, bf16[512,1536]{1,0:T(8,128)(2,1)}) custom-call(bf16[512,1536]{1,0:T(8,128)(2,1)} %get-tuple-element.157.refs_0_, bf16[512,1536]{1,0:T(8,128)(2,1)} %get-tuple-element.158.refs_1_, ...), custom_call_target="tpu_custom_call", output_to_operand_aliasing={{1}: (6, {}), {0}: (7, {})} | custom-call | flops 19327352832 | bytes 50331648 | tf_op jit(solution)/shard_map/mlp_bwd/pallas_call | solution.py:479
  775.4 36.1 %attn_bwd.5 = (bf16[4,4,512,1536]{3,2,1,0:T(8,128)(2,1)}, f32[2,512,1536]{2,1,0:T(8,128)}, f32[2,512,1536]{2,1,0:T(8,128)}) custom-call(bf16[512,1536]{1,0:T(8,128)(2,1)} %get-tuple-element.140.q_ref, bf16[512,3072]{1,0:T(8,128)(2,1)} %get-tuple-element.139.refs_3_.refs_5_.refs_7_.ko_ref.vo_ref, ...), custom_call_target="tpu_custom_call", output_to_operand_aliasing={{0}: (7, {})} | custom-call | flops 32212254720 | bytes 25165824 | tf_op jit(solution)/shard_map/attn_bwd/pallas_call | solution.py:206
  811.8 7.1 fusion.11.acc0_hbm
  822.0 14.5 d_kv.5
  836.6 34.6 %mlp_bwd.6 = (bf16[4,512,6144]{2,1,0:T(8,128)(2,1)}, bf16[2,4,512,1536]{3,2,1,0:T(8,128)(2,1)}, bf16[512,1536]{1,0:T(8,128)(2,1)}) custom-call(bf16[512,1536]{1,0:T(8,128)(2,1)} %get-tuple-element.168.refs_0_, bf16[512,1536]{1,0:T(8,128)(2,1)} %get-tuple-element.169.refs_1_, ...), custom_call_target="tpu_custom_call", output_to_operand_aliasing={{1}: (6, {}), {0}: (7, {})} | custom-call | flops 19327352832 | bytes 50331648 | tf_op jit(solution)/shard_map/mlp_bwd/pallas_call | solution.py:479
  871.1 35.9 %attn_bwd.6 = (bf16[4,4,512,1536]{3,2,1,0:T(8,128)(2,1)}, f32[2,512,1536]{2,1,0:T(8,128)}, f32[2,512,1536]{2,1,0:T(8,128)}) custom-call(bf16[512,1536]{1,0:T(8,128)(2,1)} %get-tuple-element.134.q_ref, bf16[512,3072]{1,0:T(8,128)(2,1)} %get-tuple-element.133.refs_3_.refs_5_.refs_7_.ko_ref.vo_ref, ...), custom_call_target="tpu_custom_call", output_to_operand_aliasing={{0}: (7, {})} | custom-call | flops 32212254720 | bytes 25165824 | tf_op jit(solution)/shard_map/attn_bwd/pallas_call | solution.py:206
  911.8 7.1 fusion.9.acc0_hbm
  918.9 14.6 d_kv.6
  933.4 34.1 %mlp_bwd.7 = (bf16[4,512,6144]{2,1,0:T(8,128)(2,1)}, bf16[2,4,512,1536]{3,2,1,0:T(8,128)(2,1)}, bf16[512,1536]{1,0:T(8,128)(2,1)}) custom-call(bf16[512,1536]{1,0:T(8,128)(2,1)} %get-tuple-element.179.refs_0_, bf16[512,1536]{1,0:T(8,128)(2,1)} %get-tuple-element.180.refs_1_, ...), custom_call_target="tpu_custom_call", output_to_operand_aliasing={{1}: (6, {}), {0}: (7, {})} | custom-call | flops 19327352832 | bytes 50331648 | tf_op jit(solution)/shard_map/mlp_bwd/pallas_call | solution.py:479
  967.5 19.5 %shard_map.144 = (f32[2,384,768]{2,1,0:T(8,128)}, f32[2,384,768]{2,1,0:T(8,128)}, f32[2,384,768]{2,1,0:T(8,128)}, f32[2,384,768]{2,1,0:T(8,128)}) custom-call(s32[5]{0:T(128)} %stack.40.places_ref, bf16[1,2048,6144]{2,1,0:T(8,128)(2,1)} %bitcast.64, bf16[1,2048,1536]{2,1,0:T(8,128)(2,1)} %bitcast.70), custom_call_target="tpu_custom_call" | custom-call | flops 9663676416 | bytes 18874368 | tf_op jit(solution)/shard_map/pallas_call | solution.py:324
  988.1 19.7 %shard_map.146 = (f32[2,384,768]{2,1,0:T(8,128)}, f32[2,384,768]{2,1,0:T(8,128)}, f32[2,384,768]{2,1,0:T(8,128)}, f32[2,384,768]{2,1,0:T(8,128)}) custom-call(s32[5]{0:T(128)} %stack.40.places_ref, bf16[1,2048,6144]{2,1,0:T(8,128)(2,1)} %bitcast.65, bf16[1,2048,1536]{2,1,0:T(8,128)(2,1)} %bitcast.71), custom_call_target="tpu_custom_call" | custom-call | flops 9663676416 | bytes 18874368 | tf_op jit(solution)/shard_map/pallas_call | solution.py:324
  1009.4 21.1 %shard_map.145 = (f32[2,384,768]{2,1,0:T(8,128)}, f32[2,384,768]{2,1,0:T(8,128)}, f32[2,384,768]{2,1,0:T(8,128)}, f32[2,384,768]{2,1,0:T(8,128)}) custom-call(s32[5]{0:T(128)} %stack.37.places_ref, bf16[1,2048,6144]{2,1,0:T(8,128)(2,1)} %bitcast.66, bf16[1,2048,1536]{2,1,0:T(8,128)(2,1)} %bitcast.72, f32[2,384,768]{2,1,0:T(8,128)} %collective-permute-done.33.refs_0_, ...), custom_call_target="tpu_custom_call" | custom-call | flops 9663676416 | bytes 18874368 | tf_op jit(solution)/shard_map/pallas_call | solution.py:324
  1035.5 21.1 %shard_map.147 = (f32[2,384,768]{2,1,0:T(8,128)}, f32[2,384,768]{2,1,0:T(8,128)}, f32[2,384,768]{2,1,0:T(8,128)}, f32[2,384,768]{2,1,0:T(8,128)}) custom-call(s32[5]{0:T(128)} %stack.37.places_ref, bf16[1,2048,6144]{2,1,0:T(8,128)(2,1)} %bitcast.67, bf16[1,2048,1536]{2,1,0:T(8,128)(2,1)} %bitcast.73, f32[2,384,768]{2,1,0:T(8,128)} %copy-done.15, ...), custom_call_target="tpu_custom_call" | custom-call | flops 9663676416 | bytes 18874368 | tf_op jit(solution)/shard_map/pallas_call | solution.py:324
  1056.6 35.7 %attn_bwd.7 = (bf16[4,4,512,1536]{3,2,1,0:T(8,128)(2,1)}, f32[2,512,1536]{2,1,0:T(8,128)}, f32[2,512,1536]{2,1,0:T(8,128)}) custom-call(bf16[512,1536]{1,0:T(8,128)(2,1)} %get-tuple-element.129.q_ref, bf16[512,3072]{1,0:T(8,128)(2,1)} %get-tuple-element.128.refs_3_.refs_5_.refs_7_.ko_ref.vo_ref, ...), custom_call_target="tpu_custom_call", output_to_operand_aliasing={{0}: (7, {})} | custom-call | flops 32212254720 | bytes 25165824 | tf_op jit(solution)/shard_map/attn_bwd/pallas_call | solution.py:206
  1092.7 15.6 all-to-all-done.1
  1116.3 157.8 %collective-permute-done.62 = f32[2,384,768]{2,1,0:T(8,128)S(1)} collective-permute-done((f32[2,384,768]{2,1,0:T(8,128)}, f32[2,384,768]{2,1,0:T(8,128)S(1)}, u32[]{:S(2)}, u32[]{:S(2)}) %collective-permute-start.62) | collective-permute-done | bytes 2359328 | tf_op jit(solution)/shard_map/ppermute | solution.py:31
  1285.6 14.6 d_kv.7
  1300.3 19.3 %shard_map.148 = (f32[2,384,768]{2,1,0:T(8,128)}, f32[2,384,768]{2,1,0:T(8,128)}, f32[2,384,768]{2,1,0:T(8,128)}, f32[2,384,768]{2,1,0:T(8,128)}) custom-call(s32[5]{0:T(128)} %stack.40.places_ref, bf16[4,2048,1536]{2,1,0:T(8,128)(2,1)} %bitcast.56, bf16[2,2048,1536]{2,1,0:T(8,128)(2,1)} %bitcast.60), custom_call_target="tpu_custom_call" | custom-call | flops 9663676416 | bytes 18874368 | tf_op jit(solution)/shard_map/pallas_call | solution.py:324
  1328.9 45.6 %collective-permute-done.63 = f32[2,384,768]{2,1,0:T(8,128)} collective-permute-done((f32[2,384,768]{2,1,0:T(8,128)}, f32[2,384,768]{2,1,0:T(8,128)}, u32[]{:S(2)}, u32[]{:S(2)}) %collective-permute-start.63) | collective-permute-done | bytes 2359328 | tf_op jit(solution)/shard_map/ppermute | solution.py:27
  1375.4 19.3 %shard_map.150 = (f32[2,384,768]{2,1,0:T(8,128)}, f32[2,384,768]{2,1,0:T(8,128)}, f32[2,384,768]{2,1,0:T(8,128)}, f32[2,384,768]{2,1,0:T(8,128)}) custom-call(s32[5]{0:T(128)} %stack.40.places_ref, bf16[4,2048,1536]{2,1,0:T(8,128)(2,1)} %bitcast.57, bf16[2,2048,1536]{2,1,0:T(8,128)(2,1)} %bitcast.61), custom_call_target="tpu_custom_call" | custom-call | flops 9663676416 | bytes 18874368 | tf_op jit(solution)/shard_map/pallas_call | solution.py:324
  1408.4 21.2 %shard_map.149 = (f32[2,384,768]{2,1,0:T(8,128)}, f32[2,384,768]{2,1,0:T(8,128)}, f32[2,384,768]{2,1,0:T(8,128)}, f32[2,384,768]{2,1,0:T(8,128)}) custom-call(s32[5]{0:T(128)} %stack.37.places_ref, bf16[4,2048,1536]{2,1,0:T(8,128)(2,1)} %bitcast.58, bf16[2,2048,1536]{2,1,0:T(8,128)(2,1)} %bitcast.62, f32[2,384,768]{2,1,0:T(8,128)} %copy-done.8, ...), custom_call_target="tpu_custom_call" | custom-call | flops 9663676416 | bytes 18874368 | tf_op jit(solution)/shard_map/pallas_call | solution.py:324
  1432.9 21.8 %shard_map.151 = (f32[2,384,768]{2,1,0:T(8,128)}, f32[2,384,768]{2,1,0:T(8,128)}, f32[2,384,768]{2,1,0:T(8,128)}, f32[2,384,768]{2,1,0:T(8,128)}) custom-call(s32[5]{0:T(128)} %stack.37.places_ref, bf16[4,2048,1536]{2,1,0:T(8,128)(2,1)} %bitcast.59, bf16[2,2048,1536]{2,1,0:T(8,128)(2,1)} %bitcast.63, f32[2,384,768]{2,1,0:T(8,128)} %collective-permute-done.46.refs_0_, ...), custom_call_target="tpu_custom_call" | custom-call | flops 9663676416 | bytes 18874368 | tf_op jit(solution)/shard_map/pallas_call | solution.py:324
  1454.7 10.0 fusion.2
  1464.7 16.4 fusion.24
  1482.4 10.0 fusion
  1505.8 29.4 %collective-permute-done.51 = f32[2,384,768]{2,1,0:T(8,128)S(1)} collective-permute-done((f32[2,384,768]{2,1,0:T(8,128)S(1)}, f32[2,384,768]{2,1,0:T(8,128)S(1)}, u32[]{:S(2)}, u32[]{:S(2)}) %collective-permute-start.51) | collective-permute-done | bytes 2359328 | tf_op jit(solution)/shard_map/ppermute | solution.py:27
  1538.3 16.5 fusion.25
  1559.8 21.6 %add_add_fusion.refs_0_ = f32[768,1536]{1,0:T(8,128)} fusion(f32[768,1536]{1,0:T(8,128)} %fusion.25, f32[768,1536]{1,0:T(8,128)} %fusion.24, f32[768,1536]{1,0:T(8,128)} %fusion.2, f32[768,1536]{1,0:T(8,128)} %fusion, bf16[4096,768]{1,0:T(8,128)(2,1)} %bitcast.27, bf16[4096,1536]{1,0:T(8,128)(2,1)} %all-gather.14.cloned.1.call-done), kind=kOutput, calls=%fused_computation.3 | convolution fusion | flops 9668395008 | bytes 42467328 | tf_op jit(solution)/shard_map/dot_general | solution.py:39
  1584.6 54.7 %collective-permute-done.55 = f32[2,384,768]{2,1,0:T(8,128)} collective-permute-done((f32[2,384,768]{2,1,0:T(8,128)}, f32[2,384,768]{2,1,0:T(8,128)}, u32[]{:S(2)}, u32[]{:S(2)}) %collective-permute-start.55) | collective-permute-done | bytes 2359328 | tf_op jit(solution)/shard_map/ppermute | solution.py:27
  1640.8 8.7 shard_map.153
  1656.9 18.3 %collective-permute-done.70 = bf16[512,1536]{1,0:T(8,128)(2,1)} collective-permute-done((bf16[512,1536]{1,0:T(8,128)(2,1)}, bf16[512,1536]{1,0:T(8,128)(2,1)}, u32[]{:S(2)}, u32[]{:S(2)}) %collective-permute-start.70) | collective-permute-done | bytes 1572896 | tf_op jit(solution)/shard_map/ppermute | solution.py:27
  1682.8 8.5 shard_map.152
  1691.2 10.2 shard_map.154
  (266 shorter events, 210.7 us)
Async XLA Ops:
  7.2 304.6 %all-gather.6.cloned.1.call-start = ((), (), s32[]{:S(2)}) async-start(), calls=%async_computation.4 | async-start | bytes 15925248 | tf_op jit(solution)/shard_map/all_gather | solution.py:631
  16.1 336.0 %all-gather.8.cloned.1.call-start = ((), (), s32[]{:S(2)}) async-start(), calls=%async_computation.5 | async-start | bytes 5308416 | tf_op jit(solution)/shard_map/all_gather | solution.py:631
  26.5 50.1 %collective-permute-start.2 = (bf16[384,1536]{1,0:T(8,128)(2,1)}, bf16[384,1536]{1,0:T(8,128)(2,1)}, u32[]{:S(2)}, u32[]{:S(2)}) collective-permute-start(bf16[384,1536]{1,0:T(8,128)(2,1)} %get-tuple-element.258), channel_id=1, source_target_pairs={{0,2},{2,0},{4,6},{6,4},{1,3},{3,1},{5,7},{7,5}} | collective-permute-start | bytes 3538952 | tf_op jit(solution)/shard_map/ppermute | solution.py:27
  29.9 145.5 %collective-permute-start.6 = (bf16[384,1536]{1,0:T(8,128)(2,1)}, bf16[384,1536]{1,0:T(8,128)(2,1)}, u32[]{:S(2)}, u32[]{:S(2)}) collective-permute-start(bf16[384,1536]{1,0:T(8,128)(2,1)} %get-tuple-element.258), channel_id=1, source_target_pairs={{0,4},{4,0},{2,6},{6,2},{1,5},{5,1},{3,7},{7,3}} | collective-permute-start | bytes 3538952 | tf_op jit(solution)/shard_map/ppermute | solution.py:31
  31.4 95.8 %collective-permute-start.4 = (bf16[384,1536]{1,0:T(8,128)(2,1)}, bf16[384,1536]{1,0:T(8,128)(2,1)}, u32[]{:S(2)}, u32[]{:S(2)}) collective-permute-start(bf16[384,1536]{1,0:T(8,128)(2,1)} %get-tuple-element.257), channel_id=1, source_target_pairs={{0,2},{2,0},{4,6},{6,4},{1,3},{3,1},{5,7},{7,5}} | collective-permute-start | bytes 3538952 | tf_op jit(solution)/shard_map/ppermute | solution.py:27
  34.7 131.4 %collective-permute-start.14 = (bf16[384,1536]{1,0:T(8,128)(2,1)}, bf16[384,1536]{1,0:T(8,128)(2,1)}, u32[]{:S(2)}, u32[]{:S(2)}) collective-permute-start(bf16[384,1536]{1,0:T(8,128)(2,1)} %get-tuple-element.244), channel_id=1, source_target_pairs={{0,2},{2,0},{4,6},{6,4},{1,3},{3,1},{5,7},{7,5}} | collective-permute-start | bytes 3538952 | tf_op jit(solution)/shard_map/ppermute | solution.py:27
  39.1 128.6 %collective-permute-start = (bf16[512,1536]{1,0:T(8,128)(2,1)}, bf16[512,1536]{1,0:T(8,128)(2,1)}, u32[]{:S(2)}, u32[]{:S(2)}) collective-permute-start(bf16[512,1536]{1,0:T(8,128)(2,1)} %dynamic-slice_bitcast_fusion.2), channel_id=1, source_target_pairs={{0,1},{1,0},{2,3},{3,2},{4,5},{5,4},{6,7},{7,6}} | collective-permute-start | bytes 4718600 | tf_op jit(solution)/shard_map/ppermute | solution.py:35
  40.0 1424.7 %all-gather.10.cloned.1.call-start = ((), (), s32[]{:S(2)}) async-start(), calls=%async_computation.6 | async-start | bytes 14155776 | tf_op jit(solution)/shard_map/all_gather | solution.py:631
  76.6 93.4 %collective-permute-start.3 = (bf16[384,1536]{1,0:T(8,128)(2,1)}, bf16[384,1536]{1,0:T(8,128)(2,1)S(1)}, u32[]{:S(2)}, u32[]{:S(2)}) collective-permute-start(bf16[384,1536]{1,0:T(8,128)(2,1)} %collective-permute-done.2), channel_id=1, source_target_pairs={{0,1},{1,0},{2,3},{3,2},{4,5},{5,4},{6,7},{7,6}} | collective-permute-start | bytes 3538952 | tf_op jit(solution)/shard_map/ppermute | solution.py:35
  127.2 78.0 %collective-permute-start.16 = (bf16[384,1536]{1,0:T(8,128)(2,1)S(1)}, bf16[384,1536]{1,0:T(8,128)(2,1)S(1)}, u32[]{:S(2)}, u32[]{:S(2)}) collective-permute-start(bf16[384,1536]{1,0:T(8,128)(2,1)S(1)} %get-tuple-element.243), channel_id=1, source_target_pairs={{0,2},{2,0},{4,6},{6,4},{1,3},{3,1},{5,7},{7,5}} | collective-permute-start | bytes 3538952 | tf_op jit(solution)/shard_map/ppermute | solution.py:27
  166.1 41.7 %collective-permute-start.18 = (bf16[384,1536]{1,0:T(8,128)(2,1)}, bf16[384,1536]{1,0:T(8,128)(2,1)S(1)}, u32[]{:S(2)}, u32[]{:S(2)}) collective-permute-start(bf16[384,1536]{1,0:T(8,128)(2,1)} %get-tuple-element.244), channel_id=1, source_target_pairs={{0,4},{4,0},{2,6},{6,2},{1,5},{5,1},{3,7},{7,3}} | collective-permute-start | bytes 3538952 | tf_op jit(solution)/shard_map/ppermute | solution.py:31
  167.7 41.7 %collective-permute-start.15 = (bf16[384,1536]{1,0:T(8,128)(2,1)}, bf16[384,1536]{1,0:T(8,128)(2,1)S(1)}, u32[]{:S(2)}, u32[]{:S(2)}) collective-permute-start(bf16[384,1536]{1,0:T(8,128)(2,1)} %collective-permute-done.14), channel_id=1, source_target_pairs={{0,1},{1,0},{2,3},{3,2},{4,5},{5,4},{6,7},{7,6}} | collective-permute-start | bytes 3538952 | tf_op jit(solution)/shard_map/ppermute | solution.py:35
  170.0 41.6 %collective-permute-start.5 = (bf16[384,1536]{1,0:T(8,128)(2,1)}, bf16[384,1536]{1,0:T(8,128)(2,1)S(1)}, u32[]{:S(2)}, u32[]{:S(2)}) collective-permute-start(bf16[384,1536]{1,0:T(8,128)(2,1)} %collective-permute-done.4), channel_id=1, source_target_pairs={{0,1},{1,0},{2,3},{3,2},{4,5},{5,4},{6,7},{7,6}} | collective-permute-start | bytes 3538952 | tf_op jit(solution)/shard_map/ppermute | solution.py:35
  175.4 57.6 %collective-permute-start.8 = (bf16[384,1536]{1,0:T(8,128)(2,1)}, bf16[384,1536]{1,0:T(8,128)(2,1)S(1)}, u32[]{:S(2)}, u32[]{:S(2)}) collective-permute-start(bf16[384,1536]{1,0:T(8,128)(2,1)} %get-tuple-element.257), channel_id=1, source_target_pairs={{0,4},{4,0},{2,6},{6,2},{1,5},{5,1},{3,7},{7,3}} | collective-permute-start | bytes 3538952 | tf_op jit(solution)/shard_map/ppermute | solution.py:31
  205.2 29.5 %collective-permute-start.17 = (bf16[384,1536]{1,0:T(8,128)(2,1)S(1)}, bf16[384,1536]{1,0:T(8,128)(2,1)S(1)}, u32[]{:S(2)}, u32[]{:S(2)}) collective-permute-start(bf16[384,1536]{1,0:T(8,128)(2,1)S(1)} %collective-permute-done.16), channel_id=1, source_target_pairs={{0,1},{1,0},{2,3},{3,2},{4,5},{5,4},{6,7},{7,6}} | collective-permute-start | bytes 3538952 | tf_op jit(solution)/shard_map/ppermute | solution.py:35
  207.8 50.6 %collective-permute-start.20 = (bf16[384,1536]{1,0:T(8,128)(2,1)S(1)}, bf16[384,1536]{1,0:T(8,128)(2,1)S(1)}, u32[]{:S(2)}, u32[]{:S(2)}) collective-permute-start(bf16[384,1536]{1,0:T(8,128)(2,1)S(1)} %get-tuple-element.243), channel_id=1, source_target_pairs={{0,4},{4,0},{2,6},{6,2},{1,5},{5,1},{3,7},{7,3}} | collective-permute-start | bytes 3538952 | tf_op jit(solution)/shard_map/ppermute | solution.py:31
  209.4 49.5 %collective-permute-start.7 = (bf16[384,1536]{1,0:T(8,128)(2,1)}, bf16[384,1536]{1,0:T(8,128)(2,1)S(1)}, u32[]{:S(2)}, u32[]{:S(2)}) collective-permute-start(bf16[384,1536]{1,0:T(8,128)(2,1)} %collective-permute-done.6), channel_id=1, source_target_pairs={{0,1},{1,0},{2,3},{3,2},{4,5},{5,4},{6,7},{7,6}} | collective-permute-start | bytes 3538952 | tf_op jit(solution)/shard_map/ppermute | solution.py:35
  211.6 52.2 %collective-permute-start.19 = (bf16[384,1536]{1,0:T(8,128)(2,1)S(1)}, bf16[384,1536]{1,0:T(8,128)(2,1)S(1)}, u32[]{:S(2)}, u32[]{:S(2)}) collective-permute-start(bf16[384,1536]{1,0:T(8,128)(2,1)S(1)} %collective-permute-done.18), channel_id=1, source_target_pairs={{0,1},{1,0},{2,3},{3,2},{4,5},{5,4},{6,7},{7,6}} | collective-permute-start | bytes 3538952 | tf_op jit(solution)/shard_map/ppermute | solution.py:35
  233.0 50.7 %collective-permute-start.10 = (bf16[384,1536]{1,0:T(8,128)(2,1)}, bf16[384,1536]{1,0:T(8,128)(2,1)}, u32[]{:S(2)}, u32[]{:S(2)}) collective-permute-start(bf16[384,1536]{1,0:T(8,128)(2,1)} %collective-permute-done.2), channel_id=1, source_target_pairs={{0,4},{4,0},{2,6},{6,2},{1,5},{5,1},{3,7},{7,3}} | collective-permute-start | bytes 3538952 | tf_op jit(solution)/shard_map/ppermute | solution.py:31
  234.7 31.4 %collective-permute-start.9 = (bf16[384,1536]{1,0:T(8,128)(2,1)S(1)}, bf16[384,1536]{1,0:T(8,128)(2,1)S(1)}, u32[]{:S(2)}, u32[]{:S(2)}) collective-permute-start(bf16[384,1536]{1,0:T(8,128)(2,1)S(1)} %collective-permute-done.8), channel_id=1, source_target_pairs={{0,1},{1,0},{2,3},{3,2},{4,5},{5,4},{6,7},{7,6}} | collective-permute-start | bytes 3538952 | tf_op jit(solution)/shard_map/ppermute | solution.py:35
  258.3 28.8 %collective-permute-start.12 = (bf16[384,1536]{1,0:T(8,128)(2,1)S(1)}, bf16[384,1536]{1,0:T(8,128)(2,1)S(1)}, u32[]{:S(2)}, u32[]{:S(2)}) collective-permute-start(bf16[384,1536]{1,0:T(8,128)(2,1)S(1)} %collective-permute-done.8), channel_id=1, source_target_pairs={{0,2},{2,0},{4,6},{6,4},{1,3},{3,1},{5,7},{7,5}} | collective-permute-start | bytes 3538952 | tf_op jit(solution)/shard_map/ppermute | solution.py:27
  258.9 49.5 %collective-permute-start.22 = (bf16[384,1536]{1,0:T(8,128)(2,1)}, bf16[384,1536]{1,0:T(8,128)(2,1)S(1)}, u32[]{:S(2)}, u32[]{:S(2)}) collective-permute-start(bf16[384,1536]{1,0:T(8,128)(2,1)} %collective-permute-done.14), channel_id=1, source_target_pairs={{0,4},{4,0},{2,6},{6,2},{1,5},{5,1},{3,7},{7,3}} | collective-permute-start | bytes 3538952 | tf_op jit(solution)/shard_map/ppermute | solution.py:31
  263.8 72.6 %collective-permute-start.21 = (bf16[384,1536]{1,0:T(8,128)(2,1)S(1)}, bf16[384,1536]{1,0:T(8,128)(2,1)}, u32[]{:S(2)}, u32[]{:S(2)}) collective-permute-start(bf16[384,1536]{1,0:T(8,128)(2,1)S(1)} %collective-permute-done.20), channel_id=1, source_target_pairs={{0,1},{1,0},{2,3},{3,2},{4,5},{5,4},{6,7},{7,6}} | collective-permute-start | bytes 3538952 | tf_op jit(solution)/shard_map/ppermute | solution.py:35
  266.0 74.4 %collective-permute-start.24 = (bf16[384,1536]{1,0:T(8,128)(2,1)S(1)}, bf16[384,1536]{1,0:T(8,128)(2,1)}, u32[]{:S(2)}, u32[]{:S(2)}) collective-permute-start(bf16[384,1536]{1,0:T(8,128)(2,1)S(1)} %collective-permute-done.20), channel_id=1, source_target_pairs={{0,2},{2,0},{4,6},{6,4},{1,3},{3,1},{5,7},{7,5}} | collective-permute-start | bytes 3538952 | tf_op jit(solution)/shard_map/ppermute | solution.py:27
  283.7 56.8 %collective-permute-start.11 = (bf16[384,1536]{1,0:T(8,128)(2,1)}, bf16[384,1536]{1,0:T(8,128)(2,1)}, u32[]{:S(2)}, u32[]{:S(2)}) collective-permute-start(bf16[384,1536]{1,0:T(8,128)(2,1)} %collective-permute-done.10), channel_id=1, source_target_pairs={{0,1},{1,0},{2,3},{3,2},{4,5},{5,4},{6,7},{7,6}} | collective-permute-start | bytes 3538952 | tf_op jit(solution)/shard_map/ppermute | solution.py:35
  287.1 61.5 %collective-permute-start.13 = (bf16[384,1536]{1,0:T(8,128)(2,1)S(1)}, bf16[384,1536]{1,0:T(8,128)(2,1)}, u32[]{:S(2)}, u32[]{:S(2)}) collective-permute-start(bf16[384,1536]{1,0:T(8,128)(2,1)S(1)} %collective-permute-done.12), channel_id=1, source_target_pairs={{0,1},{1,0},{2,3},{3,2},{4,5},{5,4},{6,7},{7,6}} | collective-permute-start | bytes 3538952 | tf_op jit(solution)/shard_map/ppermute | solution.py:35
  308.3 35.6 %collective-permute-start.23 = (bf16[384,1536]{1,0:T(8,128)(2,1)S(1)}, bf16[384,1536]{1,0:T(8,128)(2,1)}, u32[]{:S(2)}, u32[]{:S(2)}) collective-permute-start(bf16[384,1536]{1,0:T(8,128)(2,1)S(1)} %collective-permute-done.22), channel_id=1, source_target_pairs={{0,1},{1,0},{2,3},{3,2},{4,5},{5,4},{6,7},{7,6}} | collective-permute-start | bytes 3538952 | tf_op jit(solution)/shard_map/ppermute | solution.py:35
  740.2 798.1 %all-gather.12.cloned.1.call-start = ((), (), s32[]{:S(2)}) async-start(), calls=%async_computation.7 | async-start | bytes 14155776 | tf_op jit(solution)/shard_map/all_gather | solution.py:631
  907.9 122.6 %all-to-all-start.3 = ((bf16[8,512,768]{2,1,0:T(8,128)(2,1)}), bf16[8,512,768]{2,1,0:T(8,128)(2,1)}, u32[]{:S(2)}, u32[]{:S(2)}) async-start(bf16[8,512,768]{2,1,0:T(8,128)(2,1)} %get-tuple-element.240), calls=%async_computation.3 | async-start | bytes 12582912 | tf_op jit(solution)/shard_map/all_to_all | solution.py:673
  1007.7 26.3 %collective-permute-start.37 = (f32[2,384,768]{2,1,0:T(8,128)}, f32[2,384,768]{2,1,0:T(8,128)S(1)}, u32[]{:S(2)}, u32[]{:S(2)}) collective-permute-start(f32[2,384,768]{2,1,0:T(8,128)} %get-tuple-element.196), channel_id=1, source_target_pairs={{0,1},{1,0},{2,3},{3,2},{4,5},{5,4},{6,7},{7,6}} | collective-permute-start | bytes 7077896 | tf_op jit(solution)/shard_map/ppermute | solution.py:35
  1030.5 77.9 %all-to-all-start.1 = ((bf16[8,512,768]{2,1,0:T(8,128)(2,1)}), bf16[8,512,768]{2,1,0:T(8,128)(2,1)}, u32[]{:S(2)}, u32[]{:S(2)}) async-start(bf16[8,512,768]{2,1,0:T(8,128)(2,1)} %get-tuple-element.236), calls=%async_computation.1 | async-start | bytes 12582912 | tf_op jit(solution)/shard_map/all_to_all | solution.py:673
  1034.0 525.8 %all-gather.14.cloned.1.call-start = ((), (), s32[]{:S(2)}) async-start(), calls=%async_computation.8 | async-start | bytes 14155776 | tf_op jit(solution)/shard_map/all_gather | solution.py:631
  1092.3 193.3 %collective-permute-start.41 = (f32[2,512,1536]{2,1,0:T(8,128)}, f32[2,512,1536]{2,1,0:T(8,128)}, u32[]{:S(2)}, u32[]{:S(2)}) collective-permute-start(f32[2,512,1536]{2,1,0:T(8,128)} %get-tuple-element.208), channel_id=1, source_target_pairs={{0,1},{1,0},{2,3},{3,2},{4,5},{5,4},{6,7},{7,6}} | collective-permute-start | bytes 18874376 | tf_op jit(solution)/shard_map/ppermute | solution.py:35
  1108.4 217.0 %all-to-all-start = ((bf16[8,512,768]{2,1,0:T(8,128)(2,1)}), bf16[8,512,768]{2,1,0:T(8,128)(2,1)}, u32[]{:S(2)}, u32[]{:S(2)}) async-start(bf16[8,512,768]{2,1,0:T(8,128)(2,1)} %get-tuple-element.234), calls=%async_computation | async-start | bytes 12582912 | tf_op jit(solution)/shard_map/all_to_all | solution.py:673
  1112.2 161.9 %collective-permute-start.62 = (f32[2,384,768]{2,1,0:T(8,128)}, f32[2,384,768]{2,1,0:T(8,128)S(1)}, u32[]{:S(2)}, u32[]{:S(2)}) collective-permute-start(f32[2,384,768]{2,1,0:T(8,128)} %get-tuple-element.193), channel_id=1, source_target_pairs={{0,4},{4,0},{2,6},{6,2},{1,5},{5,1},{3,7},{7,3}} | collective-permute-start | bytes 7077896 | tf_op jit(solution)/shard_map/ppermute | solution.py:31
  1114.2 163.8 %collective-permute-start.59 = (f32[2,384,768]{2,1,0:T(8,128)}, f32[2,384,768]{2,1,0:T(8,128)S(1)}, u32[]{:S(2)}, u32[]{:S(2)}) collective-permute-start(f32[2,384,768]{2,1,0:T(8,128)} %get-tuple-element.192), channel_id=1, source_target_pairs={{0,2},{2,0},{4,6},{6,4},{1,3},{3,1},{5,7},{7,5}} | collective-permute-start | bytes 7077896 | tf_op jit(solution)/shard_map/ppermute | solution.py:27
  1115.7 209.1 %collective-permute-start.61 = (f32[2,384,768]{2,1,0:T(8,128)}, f32[2,384,768]{2,1,0:T(8,128)}, u32[]{:S(2)}, u32[]{:S(2)}) collective-permute-start(f32[2,384,768]{2,1,0:T(8,128)} %get-tuple-element.201), channel_id=1, source_target_pairs={{0,4},{4,0},{2,6},{6,2},{1,5},{5,1},{3,7},{7,3}} | collective-permute-start | bytes 7077896 | tf_op jit(solution)/shard_map/ppermute | solution.py:31
  1116.2 208.6 %collective-permute-start.58 = (f32[2,384,768]{2,1,0:T(8,128)}, f32[2,384,768]{2,1,0:T(8,128)}, u32[]{:S(2)}, u32[]{:S(2)}) collective-permute-start(f32[2,384,768]{2,1,0:T(8,128)} %get-tuple-element.190), channel_id=1, source_target_pairs={{0,2},{2,0},{4,6},{6,4},{1,3},{3,1},{5,7},{7,5}} | collective-permute-start | bytes 7077896 | tf_op jit(solution)/shard_map/ppermute | solution.py:27
  1277.5 96.9 %collective-permute-start.63 = (f32[2,384,768]{2,1,0:T(8,128)}, f32[2,384,768]{2,1,0:T(8,128)}, u32[]{:S(2)}, u32[]{:S(2)}) collective-permute-start(f32[2,384,768]{2,1,0:T(8,128)} %add.270), channel_id=1, source_target_pairs={{0,2},{2,0},{4,6},{6,4},{1,3},{3,1},{5,7},{7,5}} | collective-permute-start | bytes 7077896 | tf_op jit(solution)/shard_map/ppermute | solution.py:27
  1279.7 95.7 %collective-permute-start.60 = (f32[2,384,768]{2,1,0:T(8,128)}, f32[2,384,768]{2,1,0:T(8,128)}, u32[]{:S(2)}, u32[]{:S(2)}) collective-permute-start(f32[2,384,768]{2,1,0:T(8,128)} %add.267), channel_id=1, source_target_pairs={{0,4},{4,0},{2,6},{6,2},{1,5},{5,1},{3,7},{7,3}} | collective-permute-start | bytes 7077896 | tf_op jit(solution)/shard_map/ppermute | solution.py:31
  1319.6 75.5 %collective-permute-start.42 = (f32[2,384,768]{2,1,0:T(8,128)}, f32[2,384,768]{2,1,0:T(8,128)S(1)}, u32[]{:S(2)}, u32[]{:S(2)}) collective-permute-start(f32[2,384,768]{2,1,0:T(8,128)} %get-tuple-element.210), channel_id=1, source_target_pairs={{0,1},{1,0},{2,3},{3,2},{4,5},{5,4},{6,7},{7,6}} | collective-permute-start | bytes 7077896 | tf_op jit(solution)/shard_map/ppermute | solution.py:35
  1324.8 70.4 %collective-permute-start.43 = (f32[2,384,768]{2,1,0:T(8,128)}, f32[2,384,768]{2,1,0:T(8,128)}, u32[]{:S(2)}, u32[]{:S(2)}) collective-permute-start(f32[2,384,768]{2,1,0:T(8,128)} %get-tuple-element.211), channel_id=1, source_target_pairs={{0,1},{1,0},{2,3},{3,2},{4,5},{5,4},{6,7},{7,6}} | collective-permute-start | bytes 7077896 | tf_op jit(solution)/shard_map/ppermute | solution.py:35
  1324.8 70.7 %collective-permute-start.44 = (f32[2,384,768]{2,1,0:T(8,128)}, f32[2,384,768]{2,1,0:T(8,128)}, u32[]{:S(2)}, u32[]{:S(2)}) collective-permute-start(f32[2,384,768]{2,1,0:T(8,128)} %get-tuple-element.212), channel_id=1, source_target_pairs={{0,1},{1,0},{2,3},{3,2},{4,5},{5,4},{6,7},{7,6}} | collective-permute-start | bytes 7077896 | tf_op jit(solution)/shard_map/ppermute | solution.py:35
  1325.3 129.4 %all-to-all-start.2 = ((bf16[8,512,768]{2,1,0:T(8,128)(2,1)}), bf16[8,512,768]{2,1,0:T(8,128)(2,1)}, u32[]{:S(2)}, u32[]{:S(2)}) async-start(bf16[8,512,768]{2,1,0:T(8,128)(2,1)} %get-tuple-element.238), calls=%async_computation.2 | async-start | bytes 12582912 | tf_op jit(solution)/shard_map/all_to_all | solution.py:673
  1375.4 29.9 %collective-permute-start.45 = (f32[2,384,768]{2,1,0:T(8,128)}, f32[2,384,768]{2,1,0:T(8,128)}, u32[]{:S(2)}, u32[]{:S(2)}) collective-permute-start(f32[2,384,768]{2,1,0:T(8,128)} %get-tuple-element.213), channel_id=1, source_target_pairs={{0,1},{1,0},{2,3},{3,2},{4,5},{5,4},{6,7},{7,6}} | collective-permute-start | bytes 7077896 | tf_op jit(solution)/shard_map/ppermute | solution.py:35
  1394.7 35.0 %collective-permute-start.46 = (f32[2,384,768]{2,1,0:T(8,128)}, f32[2,384,768]{2,1,0:T(8,128)}, u32[]{:S(2)}, u32[]{:S(2)}) collective-permute-start(f32[2,384,768]{2,1,0:T(8,128)} %get-tuple-element.220), channel_id=1, source_target_pairs={{0,1},{1,0},{2,3},{3,2},{4,5},{5,4},{6,7},{7,6}} | collective-permute-start | bytes 7077896 | tf_op jit(solution)/shard_map/ppermute | solution.py:35
  1395.0 34.9 %collective-permute-start.47 = (f32[2,384,768]{2,1,0:T(8,128)}, f32[2,384,768]{2,1,0:T(8,128)}, u32[]{:S(2)}, u32[]{:S(2)}) collective-permute-start(f32[2,384,768]{2,1,0:T(8,128)} %get-tuple-element.221), channel_id=1, source_target_pairs={{0,1},{1,0},{2,3},{3,2},{4,5},{5,4},{6,7},{7,6}} | collective-permute-start | bytes 7077896 | tf_op jit(solution)/shard_map/ppermute | solution.py:35
  1395.2 35.0 %collective-permute-start.48 = (f32[2,384,768]{2,1,0:T(8,128)}, f32[2,384,768]{2,1,0:T(8,128)}, u32[]{:S(2)}, u32[]{:S(2)}) collective-permute-start(f32[2,384,768]{2,1,0:T(8,128)} %get-tuple-element.222), channel_id=1, source_target_pairs={{0,1},{1,0},{2,3},{3,2},{4,5},{5,4},{6,7},{7,6}} | collective-permute-start | bytes 7077896 | tf_op jit(solution)/shard_map/ppermute | solution.py:35
  1395.6 37.1 %collective-permute-start.49 = (f32[2,384,768]{2,1,0:T(8,128)}, f32[2,384,768]{2,1,0:T(8,128)}, u32[]{:S(2)}, u32[]{:S(2)}) collective-permute-start(f32[2,384,768]{2,1,0:T(8,128)} %get-tuple-element.223), channel_id=1, source_target_pairs={{0,1},{1,0},{2,3},{3,2},{4,5},{5,4},{6,7},{7,6}} | collective-permute-start | bytes 7077896 | tf_op jit(solution)/shard_map/ppermute | solution.py:35
  1405.3 75.9 %collective-permute-start.66 = (bf16[2048,1536]{1,0:T(8,128)(2,1)}, bf16[2048,1536]{1,0:T(8,128)(2,1)}, u32[]{:S(2)}, u32[]{:S(2)}) collective-permute-start(bf16[2048,1536]{1,0:T(8,128)(2,1)} %bitcast.24), channel_id=1, source_target_pairs={{0,1},{1,0},{2,3},{3,2},{4,5},{5,4},{6,7},{7,6}} | collective-permute-start | bytes 18874376 | tf_op jit(solution)/shard_map/ppermute | solution.py:35
  1429.6 125.2 %collective-permute-start.65 = (f32[768,768]{1,0:T(8,128)}, f32[768,768]{1,0:T(8,128)}, u32[]{:S(2)}, u32[]{:S(2)}) collective-permute-start(f32[768,768]{1,0:T(8,128)} %bitcast.22.ob_ref), channel_id=1, source_target_pairs={{0,1},{1,0},{2,3},{3,2},{4,5},{5,4},{6,7},{7,6}} | collective-permute-start | bytes 7077896 | tf_op jit(solution)/shard_map/ppermute | solution.py:35
  1430.0 129.0 %collective-permute-start.64 = (f32[768,768]{1,0:T(8,128)}, f32[768,768]{1,0:T(8,128)}, u32[]{:S(2)}, u32[]{:S(2)}) collective-permute-start(f32[768,768]{1,0:T(8,128)} %bitcast.21.oa_ref), channel_id=1, source_target_pairs={{0,1},{1,0},{2,3},{3,2},{4,5},{5,4},{6,7},{7,6}} | collective-permute-start | bytes 7077896 | tf_op jit(solution)/shard_map/ppermute | solution.py:35
  1430.2 62.2 %collective-permute-start.71 = (bf16[512,1536]{1,0:T(8,128)(2,1)S(1)}, bf16[512,1536]{1,0:T(8,128)(2,1)}, u32[]{:S(2)}, u32[]{:S(2)}) collective-permute-start(bf16[512,1536]{1,0:T(8,128)(2,1)S(1)} %get-tuple-element.254), channel_id=1, source_target_pairs={{0,2},{2,0},{5,7},{7,5}} | collective-permute-start | bytes 4718600 | tf_op jit(solution)/shard_map/ppermute | solution.py:715
  1432.7 68.8 %collective-permute-start.54 = (f32[2,384,768]{2,1,0:T(8,128)}, f32[2,384,768]{2,1,0:T(8,128)}, u32[]{:S(2)}, u32[]{:S(2)}) collective-permute-start(f32[2,384,768]{2,1,0:T(8,128)} %get-tuple-element.215), channel_id=1, source_target_pairs={{0,4},{4,0},{2,6},{6,2},{1,5},{5,1},{3,7},{7,3}} | collective-permute-start | bytes 7077896 | tf_op jit(solution)/shard_map/ppermute | solution.py:31
  1481.2 54.0 %collective-permute-start.51 = (f32[2,384,768]{2,1,0:T(8,128)S(1)}, f32[2,384,768]{2,1,0:T(8,128)S(1)}, u32[]{:S(2)}, u32[]{:S(2)}) collective-permute-start(f32[2,384,768]{2,1,0:T(8,128)S(1)} %copy-done.18), channel_id=1, source_target_pairs={{0,2},{2,0},{4,6},{6,4},{1,3},{3,1},{5,7},{7,5}} | collective-permute-start | bytes 7077896 | tf_op jit(solution)/shard_map/ppermute | solution.py:27
  1492.4 67.4 %collective-permute-start.69 = (bf16[512,1536]{1,0:T(8,128)(2,1)}, bf16[512,1536]{1,0:T(8,128)(2,1)}, u32[]{:S(2)}, u32[]{:S(2)}) collective-permute-start(bf16[512,1536]{1,0:T(8,128)(2,1)} %get-tuple-element.253), channel_id=1, source_target_pairs={{0,4},{2,6},{5,1},{7,3}} | collective-permute-start | bytes 4718600 | tf_op jit(solution)/shard_map/ppermute | solution.py:714
  1501.5 80.0 %collective-permute-start.53 = (f32[2,384,768]{2,1,0:T(8,128)}, f32[2,384,768]{2,1,0:T(8,128)}, u32[]{:S(2)}, u32[]{:S(2)}) collective-permute-start(f32[2,384,768]{2,1,0:T(8,128)} %get-tuple-element.227), channel_id=1, source_target_pairs={{0,4},{4,0},{2,6},{6,2},{1,5},{5,1},{3,7},{7,3}} | collective-permute-start | bytes 7077896 | tf_op jit(solution)/shard_map/ppermute | solution.py:31
  1535.2 118.0 %collective-permute-start.50 = (f32[2,384,768]{2,1,0:T(8,128)}, f32[2,384,768]{2,1,0:T(8,128)}, u32[]{:S(2)}, u32[]{:S(2)}) collective-permute-start(f32[2,384,768]{2,1,0:T(8,128)} %get-tuple-element.216), channel_id=1, source_target_pairs={{0,2},{2,0},{4,6},{6,4},{1,3},{3,1},{5,7},{7,5}} | collective-permute-start | bytes 7077896 | tf_op jit(solution)/shard_map/ppermute | solution.py:27
  1554.8 122.5 %collective-permute-start.72 = (bf16[1024,1536]{1,0:T(8,128)(2,1)}, bf16[1024,1536]{1,0:T(8,128)(2,1)}, u32[]{:S(2)}, u32[]{:S(2)}) collective-permute-start(bf16[1024,1536]{1,0:T(8,128)(2,1)} %pad_maximum_fusion.2), channel_id=1, source_target_pairs={{0,4},{2,6},{5,1},{7,3}} | collective-permute-start | bytes 9437192 | tf_op jit(solution)/shard_map/ppermute | solution.py:719
  1559.0 80.3 %collective-permute-start.55 = (f32[2,384,768]{2,1,0:T(8,128)}, f32[2,384,768]{2,1,0:T(8,128)}, u32[]{:S(2)}, u32[]{:S(2)}) collective-permute-start(f32[2,384,768]{2,1,0:T(8,128)} %add.264), channel_id=1, source_target_pairs={{0,2},{2,0},{4,6},{6,4},{1,3},{3,1},{5,7},{7,5}} | collective-permute-start | bytes 7077896 | tf_op jit(solution)/shard_map/ppermute | solution.py:27
  1559.8 93.4 %collective-permute-start.52 = (f32[2,384,768]{2,1,0:T(8,128)}, f32[2,384,768]{2,1,0:T(8,128)}, u32[]{:S(2)}, u32[]{:S(2)}) collective-permute-start(f32[2,384,768]{2,1,0:T(8,128)} %add.261), channel_id=1, source_target_pairs={{0,4},{4,0},{2,6},{6,2},{1,5},{5,1},{3,7},{7,3}} | collective-permute-start | bytes 7077896 | tf_op jit(solution)/shard_map/ppermute | solution.py:31
  1581.5 109.8 %collective-permute-start.67 = (f32[768,1536]{1,0:T(8,128)}, f32[768,1536]{1,0:T(8,128)}, u32[]{:S(2)}, u32[]{:S(2)}) collective-permute-start(f32[768,1536]{1,0:T(8,128)} %add_add_fusion.refs_0_), channel_id=1, source_target_pairs={{0,1},{1,0},{2,3},{3,2},{4,5},{5,4},{6,7},{7,6}} | collective-permute-start | bytes 14155784 | tf_op jit(solution)/shard_map/ppermute | solution.py:35
  1639.3 35.9 %collective-permute-start.70 = (bf16[512,1536]{1,0:T(8,128)(2,1)}, bf16[512,1536]{1,0:T(8,128)(2,1)}, u32[]{:S(2)}, u32[]{:S(2)}) collective-permute-start(bf16[512,1536]{1,0:T(8,128)(2,1)} %broadcast_select_fusion.3), channel_id=1, source_target_pairs={{0,2},{2,0},{4,6},{6,4},{1,3},{3,1},{5,7},{7,5}} | collective-permute-start | bytes 4718600 | tf_op jit(solution)/shard_map/ppermute | solution.py:27
  1653.2 28.2 %collective-permute-start.57 = (f32[2,384,768]{2,1,0:T(8,128)S(1)}, f32[2,384,768]{2,1,0:T(8,128)S(1)}, u32[]{:S(2)}, u32[]{:S(2)}) collective-permute-start(f32[2,384,768]{2,1,0:T(8,128)S(1)} %add_add_fusion.3.own_b), channel_id=1, source_target_pairs={{0,1},{1,0},{2,3},{3,2},{4,5},{5,4},{6,7},{7,6}} | collective-permute-start | bytes 7077896 | tf_op jit(solution)/shard_map/ppermute | solution.py:35
  (43 other events, 1096.1 us)
Sparse Core Ops, SparseCore 0:
  16.2 129.7 all-gather.5
  148.4 52.1 all-gather.7
  740.3 66.2 all-gather.9
  836.7 65.9 all-gather.11
  1092.9 149.7 all-gather.13

commit v11 on v10

--- a/solution.py
+++ b/solution.py
@@ -303,61 +303,60 @@
 
 
 def terms_body(added, slot_of, places_ref, lhs_ref, rhs_ref, *refs):
-    recv, outs = refs[:4 * added], refs[-4:]
+    count = len(refs) // (1 + added)
+    recv, outs = refs[:count * added], refs[-count:]
     step = pl.program_id(0)
     val = tn(lhs_ref[0], rhs_ref[0])
-    for slot in range(4):
+    for slot in range(count):
         @pl.when(slot_of(step) == slot)
         def _():
             outs[slot][0] = val + recv[slot][0] if added else val
 
 
-def terms(lhs, rhs, rows, cols, places, plan, chips, recv):
+def terms(lhs, rhs, rows, cols, places, plans, chips, recv):
     tokens = lhs.shape[1]
-    first, second = chips
-    lhs_at, rhs_at, slot_of, turns = plan
+    lhs_at, rhs_at, slot_of, turns = plans[len(chips) - 1]
 
     def rel(r):
-        return first + r * (second - first)
+        return chips[0] + r * (chips[-1] - chips[0])
 
     slots = [pl.BlockSpec((1, rows, cols), lambda i, p, at=at: (jnp.clip(i - at, 0, 1), 0, 0)) for at in turns]
     out = pl.pallas_call(
-        functools.partial(terms_body, len(recv) // 4, slot_of),
+        functools.partial(terms_body, int(bool(recv)), slot_of),
         grid_spec=pltpu.PrefetchScalarGridSpec(
-            num_scalar_prefetch=1, grid=(8,),
+            num_scalar_prefetch=1, grid=(4 * len(chips),),
             in_specs=[pl.BlockSpec((1, tokens, rows), lambda i, p: lhs_at(i, rel, p)),
                       pl.BlockSpec((1, tokens, cols), lambda i, p: rhs_at(i, p))] + slots[:len(recv)],
             out_specs=slots),
-        out_shape=[jax.ShapeDtypeStruct((2, rows, cols), F32)] * 4,
+        out_shape=[jax.ShapeDtypeStruct((2, rows, cols), F32)] * len(turns),
         compiler_params=pltpu.CompilerParams(dimension_semantics=('arbitrary',), vmem_limit_bytes=VMEM_ALL),
-        cost_estimate=pl.CostEstimate(flops=16 * tokens * rows * cols, bytes_accessed=24 * tokens * rows, transcendentals=0),
+        cost_estimate=pl.CostEstimate(flops=8 * len(chips) * tokens * rows * cols, bytes_accessed=24 * tokens * rows,
+                                      transcendentals=0),
     )(places, lhs, rhs, *recv)
-    return {first: out[:2], second: out[2:]}
-
-
-ATTN_PLAN = (lambda i, rel, p: (jnp.where(i < 4, i % 2, i // 2), 0, rel(jnp.where(i < 4, i // 2, i % 2))),
-             lambda i, p: (i // 6, 0, p[0]),
-             lambda i: jnp.where(i < 4, 2 * (i // 2), 2 * (i % 2) + 1),
-             (0, 5, 2, 6))
-UP_PLAN = (lambda i, rel, p: (0, 0, 4 * p[1 + rel((i // 2) % 2)] + 2 * p[0] + i % 2),
-           lambda i, p: (0, 0, i // 4),
-           lambda i: 2 * ((i // 2) % 2) + i // 4,
-           (0, 4, 2, 6))
-
-
-def summed_terms(lhs, rhs, rows, cols, places, plan):
-    def in_turn(where, done):
+    return {chip: out[2 * n:2 * n + 2] for n, chip in enumerate(chips)}
+
+
+ATTN_PLANS = (
+    (lambda i, rel, p: (i, 0, rel(0)), lambda i, p: (i // 3, 0, p[0]), lambda i: i // 2, (0, 2)),
+    (lambda i, rel, p: (jnp.where(i < 4, i % 2, i // 2), 0, rel(jnp.where(i < 4, i // 2, i % 2))),
+     lambda i, p: (i // 6, 0, p[0]), lambda i: jnp.where(i < 4, 2 * (i // 2), 2 * (i % 2) + 1), (0, 5, 2, 6)))
+UP_PLANS = (
+    (lambda i, rel, p: (0, 0, 4 * p[1 + rel(0)] + 2 * p[0] + i % 2), lambda i, p: (0, 0, i // 2), lambda i: i // 2, (0, 2)),
+    (lambda i, rel, p: (0, 0, 4 * p[1 + rel((i // 2) % 2)] + 2 * p[0] + i % 2),
+     lambda i, p: (0, 0, i // 4), lambda i: 2 * ((i // 2) % 2) + i // 4, (0, 4, 2, 6)))
+
+
+def summed_terms(operands, places, plans, groups, done=()):
+    def in_turn(where):
         return lax.optimization_barrier((where, done))[0] if done else where
 
     sent, total = {}, {}
-    where, done = places[1], []
-    for pair in ((3, 1), (2, 0)):
-        out = terms(lhs, rhs, rows, cols, in_turn(where, done), plan, pair, [])
+    for group in groups:
+        out = terms(*operands, in_turn(places[1]), plans, group, [])
         done = [v for ab in out.values() for v in ab]
         sent.update({r: [pp_d(v) for v in ab] for r, ab in out.items()})
-    where, done = places[0], []
-    for pair in ((3, 1), (2, 0)):
-        out = terms(lhs, rhs, rows, cols, in_turn(where, done), plan, pair, sent[pair[0]] + sent[pair[1]])
+    for group in groups:
+        out = terms(*operands, in_turn(places[0]), plans, group, [v for r in group for v in sent[r]])
         done = [v for ab in out.values() for v in ab]
         total.update(out)
     return total
@@ -370,12 +369,21 @@
 
 
 def mlp_fwd_body(*refs):
-    x0_ref, e_ref, ctx_ref, wo_ref, w1_ref, w2_ref = refs[:6]
-    z_ref, g_ref, x_ref, h_ref, m_ref, acc_ref = refs[-6:]
+    x0_ref, e_ref, ctx_ref, wo_ref, w1_hbm, w2_hbm = refs[:6]
+    z_ref, g_ref, x_ref, h_ref, m_ref, acc_ref, w1_ref, w2_ref, sems = refs[-9:]
     j = pl.program_id(0)
+    last = pl.num_programs(0) - 1
+
+    def fetch(step):
+        rows = pl.ds(pl.multiple_of(step * BLOCK_F, BLOCK_F), BLOCK_F)
+        slot = step % 2
+        return [pltpu.make_async_copy(hbm.at[rows], ref.at[slot], sems.at[n, slot])
+                for n, (hbm, ref) in enumerate(((w1_hbm, w1_ref), (w2_hbm, w2_ref)))]
 
     @pl.when(j == 0)
     def _():
+        for copy in fetch(0):
+            copy.start()
         for rows in ROWS:
             s = x0_ref[rows, :].astype(F32) + e_ref[...]
             h = (s + nn(ctx_ref[0, 0, rows, :], wo_ref[...])).astype(BF16)
@@ -384,17 +392,25 @@
             acc_ref[rows, :] = hf
             m_ref[0, rows, :] = (hf * lax.rsqrt(jnp.mean(hf * hf, axis=-1, keepdims=True) + EPS_NORM)).astype(BF16)
 
+    @pl.when(j < last)
+    def _():
+        for copy in fetch(j + 1):
+            copy.start()
+
+    for copy in fetch(j):
+        copy.wait()
+    slot = j % 2
     for rows in ROWS:
-        z = nt(m_ref[0, rows, :], w1_ref[...]).astype(BF16)
+        z = nt(m_ref[0, rows, :], w1_ref[slot]).astype(BF16)
         z_ref[rows, :] = z
         zf = z.astype(F32)
         t = jnp.tanh(zf * (GELU_C + (GELU_A * GELU_C) * (zf * zf)))
         half = 0.5 * zf
         g_ref[0, rows, :] = (half + half * t).astype(BF16)
     for rows in ROWS:
-        acc_ref[rows, :] += nn(g_ref[0, rows, :], w2_ref[...])
-
-    @pl.when(j == pl.num_programs(0) - 1)
+        acc_ref[rows, :] += nn(g_ref[0, rows, :], w2_ref[slot])
+
+    @pl.when(j == last)
     def _():
         x_ref[...] = acc_ref[...].astype(BF16)
 
@@ -404,21 +420,21 @@
     hidden = w2.shape[0]
     whole = pl.BlockSpec((t, dim), lambda j: (0, 0))
     slab = pl.BlockSpec((1, t, dim), lambda j: (layer, 0, 0))
-    wblk = pl.BlockSpec((BLOCK_F, dim), lambda j: (j, 0))
+    hbm = pl.BlockSpec(memory_space=pl.ANY)
     extra = [] if hist is None else [hist]
     return pl.pallas_call(
         mlp_fwd_body,
         grid=(hidden // BLOCK_F,),
         in_specs=[whole, pl.BlockSpec((1, dim), lambda j: (0, 0)), pl.BlockSpec((1, 1, t, dim), lambda j: (3, layer, 0, 0)),
-                  pl.BlockSpec((dim, dim), lambda j: (0, 0)), wblk, wblk]
-        + [pl.BlockSpec(memory_space=pl.ANY)] * len(extra),
+                  pl.BlockSpec((dim, dim), lambda j: (0, 0)), hbm, hbm] + [hbm] * len(extra),
         out_specs=[pl.BlockSpec((t, BLOCK_F), lambda j: (0, j)),
                    pl.BlockSpec((1, t, BLOCK_F), lambda j: (j, 0, 0)), whole, whole, slab],
         out_shape=[jax.ShapeDtypeStruct((t, hidden), BF16),
                    jax.ShapeDtypeStruct((hidden // BLOCK_F, t, BLOCK_F), BF16),
                    jax.ShapeDtypeStruct((t, dim), BF16), jax.ShapeDtypeStruct((t, dim), BF16),
                    jax.ShapeDtypeStruct((layers, t, dim), BF16)],
-        scratch_shapes=[pltpu.VMEM((t, dim), F32)],
+        scratch_shapes=[pltpu.VMEM((t, dim), F32), pltpu.VMEM((2, BLOCK_F, dim), BF16), pltpu.VMEM((2, BLOCK_F, dim), BF16),
+                        pltpu.SemaphoreType.DMA((2, 2))],
         input_output_aliases={6: 4} if extra else {},
         compiler_params=pltpu.CompilerParams(dimension_semantics=('arbitrary',), vmem_limit_bytes=VMEM_ALL),
         cost_estimate=pl.CostEstimate(flops=4 * t * dim * hidden, bytes_accessed=4 * dim * hidden + 4 * t * hidden,
@@ -688,18 +704,27 @@
                 next_all[layer] = gather(d_next)
             up_hist, um_hist, d_ctx = mlp_bwd(d_next, h, z, wo, w1, w2, layer, layer_count, um_hist, up_hist)
             if layer == 0:
-                total = summed_terms(flat(up_hist, 1), flat(m_hist, 1), hid, half_d, places, UP_PLAN)
-                d_ctx = after(d_ctx, *[v for r in (1, 2, 3) for v in total[r]])
-                own_1a = reduce_terms({r: v[0] for r, v in total.items()}, pp_x, pp_y, 1, 2)
-                own_1b = reduce_terms({r: v[1] for r, v in total.items()}, pp_y, pp_x, 2, 1)
+                up_operands = (flat(up_hist, 1), flat(m_hist, 1), hid, half_d)
+                up_total = summed_terms(up_operands, places, UP_PLANS, ((3, 1), (2,)))
+                d_ctx = after(d_ctx, *[v for ab in up_total.values() for v in ab])
             att_hist, own_kv, sib_kv = attn_bwd(q, kv, kv_s, d_ctx, lse, layer, layer_count, att_hist)
             recv_kv = pp_d(sib_kv)
             acc0 = nn(att_hist[0, layer], wq)
             att_hist, d_cur = d_kv(acc0, x_l, e, um_hist, own_kv, recv_kv, wkv, layer, layer_count, att_hist)
 
-        total = summed_terms(flat(att_hist, 4), flat(um_hist, 2), hid, half_d, places, ATTN_PLAN)
-        own_qk = reduce_terms({r: v[0] for r, v in total.items()}, pp_x, pp_y, 1, 2)
-        own_vo = reduce_terms({r: v[1] for r, v in total.items()}, pp_y, pp_x, 2, 1)
+        att_operands = (flat(att_hist, 4), flat(um_hist, 2), hid, half_d)
+        att_total = summed_terms(att_operands, places, ATTN_PLANS, ((3, 1), (2,)))
+        ready = [v for ab in att_total.values() for v in ab]
+        att_total.update(summed_terms(att_operands, places, ATTN_PLANS, ((0,),), ready))
+        up_total.update(summed_terms(up_operands, places, UP_PLANS, ((0,),), ready))
+
+        def part(total, n):
+            return {r: ab[n] for r, ab in total.items()}
+
+        own_1a = reduce_terms(part(up_total, 0), pp_x, pp_y, 1, 2)
+        own_1b = reduce_terms(part(up_total, 1), pp_y, pp_x, 2, 1)
+        own_qk = reduce_terms(part(att_total, 0), pp_x, pp_y, 1, 2)
+        own_vo = reduce_terms(part(att_total, 1), pp_y, pp_x, 2, 1)
 
         at_home = chip_y == core
         to_row = [(2 * c + d, 2 * (c ^ 2) + d) for c in range(4) for d in range(2) if c // 2 == d]
@@ -721,7 +746,6 @@
         p_0, p_1 = in_order(p_row, p_x)
         d_x = jnp.concatenate([p_0, q_both[:half_t], p_1, q_both[half_t:]], axis=0).reshape(2, -1, dim)
 
-        ready = tuple(v for ab in total.values() for v in ab)
         cot_mine = cot_out.reshape(-1, dim)
         cot_other = pp_d(cot_mine)
         grad_2 = None

time: 1720 us -> 1780 us (1.035)
  waiting for transfers between devices: 564 us -> 602 us
    all_to_all x4, waiting for transfers between devices: 15.6 us -> 157 us  [device_step(): lax.all_to_all(g.reshape(-1, g.shape[-1]), BOTH, split_axis=0, concat_axi...]
    ppermute x12, waiting for transfers between devices: 241 us -> 161 us  [pp_y(): return lax.ppermute(v, 'model', SWAP_Y)]
    ppermute x13, waiting for transfers between devices: 283 us -> 224 us  [pp_x(): return lax.ppermute(v, 'model', SWAP_X)]
    ppermute x1, waiting for transfers between devices: 0.01 us -> 33.7 us  [device_step(): q_x = lax.ppermute(part_q, BOTH, in_row)]
    pallas_call x8 -> x12, Pallas kernels: 163 us -> 179 us  [terms(): pl.pallas_call(functools.partial(terms_body, int(bool(recv)), slot_of), g...]
  transfers between devices with their start and end apart: 82 -> 82, of which waited for: 22 -> 27; matrix products, arithmetic and copies ran while one was open for 14% -> 14% of each run, Pallas kernels for 27% -> 27%
where the time goes in v11:
time: 1780 us; the launch traced here: 1770 us
  Pallas kernels  830 us (47%)
  waiting for transfers between devices  602 us (34%)
  matrix products  103 us (6%)
  local copies, waits for them, and re-layouts  92.2 us (5%)
  starting transfers between devices  67.7 us (4%)
  other arithmetic  59.9 us (3%)
    ppermute x13, waiting for transfers between devices, pp_x(): return lax.ppermute(v, 'model', SWAP_X)  224 us
    pallas_call x12, Pallas kernels, terms(): pl.pallas_call(functools.partial(terms_body, int(bool(recv)), slot_of), g...  179 us
    ppermute x12, waiting for transfers between devices, pp_y(): return lax.ppermute(v, 'model', SWAP_Y)  161 us
    all_to_all x4, waiting for transfers between devices, device_step(): lax.all_to_all(g.reshape(-1, g.shape[-1]), BOTH, split_axis=0, concat_axi...  157 us
    pallas_call x4, Pallas kernels, attn_bwd(): pl.pallas_call(attn_bwd_body, grid=(steps,), in_specs=[qblk, kblk, kblk,...  144 us
    pallas_call x4, Pallas kernels, mlp_bwd(): pl.pallas_call(mlp_bwd_body, grid=(hidden // BLOCK_B,), in_specs=[whole,...  138 us
    pallas_call x4, Pallas kernels, mlp_fwd(): pl.pallas_call(mlp_fwd_body, grid=(hidden // BLOCK_F,), in_specs=[whole,...  130 us
    dot_general x9, matrix products, dot(): return lax.dot_general(a, b, (dims, ((), ())), preferred_element_type=F32)  103 us
  transfers between devices with their start and end apart: 82, of which 27 were waited for; matrix products, arithmetic and copies ran while one was open for 14% of the time, Pallas kernels for 27%

profile of v11, /device:TPU:0, one launch (start us, length us, event | category | flops | bytes accessed | tf_op | source)
XLA Modules:
  0.0 1769.6 jit_solution(15001245400175519868)
XLA Ops:
  41.0 7.3 broadcast.6.clone
  52.0 24.6 %collective-permute-done.2 = bf16[384,1536]{1,0:T(8,128)(2,1)} collective-permute-done((bf16[384,1536]{1,0:T(8,128)(2,1)}, bf16[384,1536]{1,0:T(8,128)(2,1)}, u32[]{:S(2)}, u32[]{:S(2)}) %collective-permute-start.2) | collective-permute-done | bytes 1179680 | tf_op jit(solution)/shard_map/ppermute | solution.py:27
  86.1 41.1 %collective-permute-done.4 = bf16[384,1536]{1,0:T(8,128)(2,1)} collective-permute-done((bf16[384,1536]{1,0:T(8,128)(2,1)}, bf16[384,1536]{1,0:T(8,128)(2,1)}, u32[]{:S(2)}, u32[]{:S(2)}) %collective-permute-start.4) | collective-permute-done | bytes 1179680 | tf_op jit(solution)/shard_map/ppermute | solution.py:27
  130.1 35.9 %collective-permute-done.14 = bf16[384,1536]{1,0:T(8,128)(2,1)} collective-permute-done((bf16[384,1536]{1,0:T(8,128)(2,1)}, bf16[384,1536]{1,0:T(8,128)(2,1)}, u32[]{:S(2)}, u32[]{:S(2)}) %collective-permute-start.14) | collective-permute-done | bytes 1179680 | tf_op jit(solution)/shard_map/ppermute | solution.py:27
  175.7 29.5 %collective-permute-done.16 = bf16[384,1536]{1,0:T(8,128)(2,1)S(1)} collective-permute-done((bf16[384,1536]{1,0:T(8,128)(2,1)S(1)}, bf16[384,1536]{1,0:T(8,128)(2,1)S(1)}, u32[]{:S(2)}, u32[]{:S(2)}) %collective-permute-start.16) | collective-permute-done | bytes 1179680 | tf_op jit(solution)/shard_map/ppermute | solution.py:27
  215.6 17.4 collective-permute-done.8
  235.8 22.5 %collective-permute-done.20 = bf16[384,1536]{1,0:T(8,128)(2,1)S(1)} collective-permute-done((bf16[384,1536]{1,0:T(8,128)(2,1)S(1)}, bf16[384,1536]{1,0:T(8,128)(2,1)S(1)}, u32[]{:S(2)}, u32[]{:S(2)}) %collective-permute-start.20) | collective-permute-done | bytes 1179680 | tf_op jit(solution)/shard_map/ppermute | solution.py:31
  267.5 16.2 collective-permute-done.10
  287.1 21.2 %collective-permute-done.22 = bf16[384,1536]{1,0:T(8,128)(2,1)S(1)} collective-permute-done((bf16[384,1536]{1,0:T(8,128)(2,1)}, bf16[384,1536]{1,0:T(8,128)(2,1)S(1)}, u32[]{:S(2)}, u32[]{:S(2)}) %collective-permute-start.22) | collective-permute-done | bytes 1179680 | tf_op jit(solution)/shard_map/ppermute | solution.py:31
  311.8 14.8 spread.1
  326.6 9.9 norm_kv.4
  357.4 24.9 %attn_fwd.4 = (bf16[512,1536]{1,0:T(8,128)(2,1)}, bf16[4,4,512,1536]{3,2,1,0:T(8,128)(2,1)}, f32[12,2,512]{2,1,0:T(2,128)}) custom-call(bf16[2,4,512,1536]{3,2,1,0:T(8,128)(2,1)} %get-tuple-element.131.refs_0_.refs_3_, bf16[1536,1536]{1,0:T(8,128)(2,1)} %get-tuple-element.132.refs_1_.refs_2_, bf16[1536,1536]{1,0:T(8,128)(2,1)} %get-tuple-element.132.refs_1_.refs_2_, ...), custom_call_target="tpu_custom_call" | custom-call | flops 12884901888 | bytes 9437184 | tf_op jit(solution)/shard_map/attn_fwd/pallas_call | solution.py:125
  382.3 32.4 %mlp_fwd.4 = (bf16[512,6144]{1,0:T(8,128)(2,1)}, bf16[8,512,768]{2,1,0:T(8,128)(2,1)}, bf16[512,1536]{1,0:T(8,128)(2,1)}, bf16[512,1536]{1,0:T(8,128)(2,1)}, bf16[4,512,1536]{2,1,0:T(8,128)(2,1)}) custom-call(bf16[512,1536]{1,0:T(8,128)(2,1)} %bitcast_select_fusion.1.refs_0_.x_hbm, f32[1,1536]{1,0:T(1,128)} %get-tuple-element.272.refs_1_.e_ref, ...), custom_call_target="tpu_custom_call" | custom-call | flops 19327352832 | bytes 50331648 | tf_op jit(solution)/shard_map/mlp_fwd/pallas_call | solution.py:425
  414.7 9.9 norm_kv.5
  430.8 24.9 %attn_fwd.5 = (bf16[512,1536]{1,0:T(8,128)(2,1)}, bf16[4,4,512,1536]{3,2,1,0:T(8,128)(2,1)}, f32[12,2,512]{2,1,0:T(2,128)}) custom-call(bf16[2,4,512,1536]{3,2,1,0:T(8,128)(2,1)} %get-tuple-element.137.refs_0_.refs_3_, bf16[1536,1536]{1,0:T(8,128)(2,1)} %get-tuple-element.132.refs_1_.refs_2_, ...), custom_call_target="tpu_custom_call", output_to_operand_aliasing={{1}: (9, {})} | custom-call | flops 12884901888 | bytes 9437184 | tf_op jit(solution)/shard_map/attn_fwd/pallas_call | solution.py:125
  455.7 32.5 %mlp_fwd.5 = (bf16[512,6144]{1,0:T(8,128)(2,1)}, bf16[8,512,768]{2,1,0:T(8,128)(2,1)}, bf16[512,1536]{1,0:T(8,128)(2,1)}, bf16[512,1536]{1,0:T(8,128)(2,1)}, bf16[4,512,1536]{2,1,0:T(8,128)(2,1)}) custom-call(bf16[512,1536]{1,0:T(8,128)(2,1)} %get-tuple-element.136.refs_0_.x_hbm, ...), custom_call_target="tpu_custom_call", output_to_operand_aliasing={{4}: (6, {})} | custom-call | flops 19327352832 | bytes 50331648 | tf_op jit(solution)/shard_map/mlp_fwd/pallas_call | solution.py:425
  488.2 9.9 norm_kv.6
  504.1 24.9 %attn_fwd.6 = (bf16[512,1536]{1,0:T(8,128)(2,1)}, bf16[4,4,512,1536]{3,2,1,0:T(8,128)(2,1)}, f32[12,2,512]{2,1,0:T(2,128)}) custom-call(bf16[2,4,512,1536]{3,2,1,0:T(8,128)(2,1)} %get-tuple-element.143.refs_0_.refs_3_, bf16[1536,1536]{1,0:T(8,128)(2,1)} %get-tuple-element.132.refs_1_.refs_2_, ...), custom_call_target="tpu_custom_call", output_to_operand_aliasing={{1}: (9, {})} | custom-call | flops 12884901888 | bytes 9437184 | tf_op jit(solution)/shard_map/attn_fwd/pallas_call | solution.py:125
  529.0 32.5 %mlp_fwd.6 = (bf16[512,6144]{1,0:T(8,128)(2,1)}, bf16[8,512,768]{2,1,0:T(8,128)(2,1)}, bf16[512,1536]{1,0:T(8,128)(2,1)}, bf16[512,1536]{1,0:T(8,128)(2,1)}, bf16[4,512,1536]{2,1,0:T(8,128)(2,1)}) custom-call(bf16[512,1536]{1,0:T(8,128)(2,1)} %get-tuple-element.142.refs_0_.x_hbm, ...), custom_call_target="tpu_custom_call", output_to_operand_aliasing={{4}: (6, {})} | custom-call | flops 19327352832 | bytes 50331648 | tf_op jit(solution)/shard_map/mlp_fwd/pallas_call | solution.py:425
  561.5 9.9 norm_kv.7
  582.6 24.9 %attn_fwd.7 = (bf16[512,1536]{1,0:T(8,128)(2,1)}, bf16[4,4,512,1536]{3,2,1,0:T(8,128)(2,1)}, f32[12,2,512]{2,1,0:T(2,128)}) custom-call(bf16[2,4,512,1536]{3,2,1,0:T(8,128)(2,1)} %get-tuple-element.149.refs_0_.refs_6_, bf16[1536,1536]{1,0:T(8,128)(2,1)} %get-tuple-element.132.refs_1_.refs_2_, ...), custom_call_target="tpu_custom_call", output_to_operand_aliasing={{1}: (9, {})} | custom-call | flops 12884901888 | bytes 9437184 | tf_op jit(solution)/shard_map/attn_fwd/pallas_call | solution.py:125
  607.5 32.4 %mlp_fwd.7 = (bf16[512,6144]{1,0:T(8,128)(2,1)}, bf16[8,512,768]{2,1,0:T(8,128)(2,1)}, bf16[512,1536]{1,0:T(8,128)(2,1)}, bf16[512,1536]{1,0:T(8,128)(2,1)}, bf16[4,512,1536]{2,1,0:T(8,128)(2,1)}) custom-call(bf16[512,1536]{1,0:T(8,128)(2,1)} %get-tuple-element.148.refs_0_.x_hbm, ...), custom_call_target="tpu_custom_call", output_to_operand_aliasing={{4}: (6, {})} | custom-call | flops 19327352832 | bytes 50331648 | tf_op jit(solution)/shard_map/mlp_fwd/pallas_call | solution.py:425
  639.9 34.0 %mlp_bwd.4 = (bf16[4,512,6144]{2,1,0:T(8,128)(2,1)}, bf16[2,4,512,1536]{3,2,1,0:T(8,128)(2,1)}, bf16[512,1536]{1,0:T(8,128)(2,1)}) custom-call(bf16[512,1536]{1,0:T(8,128)(2,1)} %bitcast_select_fusion.refs_0_, bf16[512,1536]{1,0:T(8,128)(2,1)} %get-tuple-element.154.refs_1_, ...), custom_call_target="tpu_custom_call", output_to_operand_aliasing={{1}: (6, {})} | custom-call | flops 19327352832 | bytes 50331648 | tf_op jit(solution)/shard_map/mlp_bwd/pallas_call | solution.py:495
  673.9 36.1 %attn_bwd.4 = (bf16[4,4,512,1536]{3,2,1,0:T(8,128)(2,1)}, f32[2,512,1536]{2,1,0:T(8,128)}, f32[2,512,1536]{2,1,0:T(8,128)}) custom-call(bf16[512,1536]{1,0:T(8,128)(2,1)} %get-tuple-element.151.q_ref, bf16[512,3072]{1,0:T(8,128)(2,1)} %get-tuple-element.150.refs_3_.refs_5_.refs_7_.ko_ref.vo_ref, ...), custom_call_target="tpu_custom_call", output_to_operand_aliasing={{0}: (7, {})} | custom-call | flops 32212254720 | bytes 25165824 | tf_op jit(solution)/shard_map/attn_bwd/pallas_call | solution.py:206
  720.5 14.5 d_kv.4
  735.1 35.1 %mlp_bwd.5 = (bf16[4,512,6144]{2,1,0:T(8,128)(2,1)}, bf16[2,4,512,1536]{3,2,1,0:T(8,128)(2,1)}, bf16[512,1536]{1,0:T(8,128)(2,1)}) custom-call(bf16[512,1536]{1,0:T(8,128)(2,1)} %get-tuple-element.162.refs_0_, bf16[512,1536]{1,0:T(8,128)(2,1)} %get-tuple-element.163.refs_1_, ...), custom_call_target="tpu_custom_call", output_to_operand_aliasing={{1}: (6, {}), {0}: (7, {})} | custom-call | flops 19327352832 | bytes 50331648 | tf_op jit(solution)/shard_map/mlp_bwd/pallas_call | solution.py:495
  770.3 36.0 %attn_bwd.5 = (bf16[4,4,512,1536]{3,2,1,0:T(8,128)(2,1)}, f32[2,512,1536]{2,1,0:T(8,128)}, f32[2,512,1536]{2,1,0:T(8,128)}) custom-call(bf16[512,1536]{1,0:T(8,128)(2,1)} %get-tuple-element.145.q_ref, bf16[512,3072]{1,0:T(8,128)(2,1)} %get-tuple-element.144.refs_3_.refs_5_.refs_7_.ko_ref.vo_ref, ...), custom_call_target="tpu_custom_call", output_to_operand_aliasing={{0}: (7, {})} | custom-call | flops 32212254720 | bytes 25165824 | tf_op jit(solution)/shard_map/attn_bwd/pallas_call | solution.py:206
  816.8 14.5 d_kv.5
  831.3 34.6 %mlp_bwd.6 = (bf16[4,512,6144]{2,1,0:T(8,128)(2,1)}, bf16[2,4,512,1536]{3,2,1,0:T(8,128)(2,1)}, bf16[512,1536]{1,0:T(8,128)(2,1)}) custom-call(bf16[512,1536]{1,0:T(8,128)(2,1)} %get-tuple-element.173.refs_0_, bf16[512,1536]{1,0:T(8,128)(2,1)} %get-tuple-element.174.refs_1_, ...), custom_call_target="tpu_custom_call", output_to_operand_aliasing={{1}: (6, {}), {0}: (7, {})} | custom-call | flops 19327352832 | bytes 50331648 | tf_op jit(solution)/shard_map/mlp_bwd/pallas_call | solution.py:495
  865.9 36.2 %attn_bwd.6 = (bf16[4,4,512,1536]{3,2,1,0:T(8,128)(2,1)}, f32[2,512,1536]{2,1,0:T(8,128)}, f32[2,512,1536]{2,1,0:T(8,128)}) custom-call(bf16[512,1536]{1,0:T(8,128)(2,1)} %get-tuple-element.139.q_ref, bf16[512,3072]{1,0:T(8,128)(2,1)} %get-tuple-element.138.refs_3_.refs_5_.refs_7_.ko_ref.vo_ref, ...), custom_call_target="tpu_custom_call", output_to_operand_aliasing={{0}: (7, {})} | custom-call | flops 32212254720 | bytes 25165824 | tf_op jit(solution)/shard_map/attn_bwd/pallas_call | solution.py:206
  902.9 7.1 fusion.9.acc0_hbm
  912.6 14.5 d_kv.6
  927.1 34.4 %mlp_bwd.7 = (bf16[4,512,6144]{2,1,0:T(8,128)(2,1)}, bf16[2,4,512,1536]{3,2,1,0:T(8,128)(2,1)}, bf16[512,1536]{1,0:T(8,128)(2,1)}) custom-call(bf16[512,1536]{1,0:T(8,128)(2,1)} %get-tuple-element.184.refs_0_, bf16[512,1536]{1,0:T(8,128)(2,1)} %get-tuple-element.185.refs_1_, ...), custom_call_target="tpu_custom_call", output_to_operand_aliasing={{1}: (6, {}), {0}: (7, {})} | custom-call | flops 19327352832 | bytes 50331648 | tf_op jit(solution)/shard_map/mlp_bwd/pallas_call | solution.py:495
  961.5 19.6 %shard_map.144 = (f32[2,384,768]{2,1,0:T(8,128)}, f32[2,384,768]{2,1,0:T(8,128)}, f32[2,384,768]{2,1,0:T(8,128)}, f32[2,384,768]{2,1,0:T(8,128)}) custom-call(s32[5]{0:T(128)} %stack.39.places_ref, bf16[1,2048,6144]{2,1,0:T(8,128)(2,1)} %bitcast.68, bf16[1,2048,1536]{2,1,0:T(8,128)(2,1)} %bitcast.74), custom_call_target="tpu_custom_call" | custom-call | flops 9663676416 | bytes 18874368 | tf_op jit(solution)/shard_map/pallas_call | solution.py:324
  982.1 11.9 shard_map.145
  998.8 21.1 %shard_map.146 = (f32[2,384,768]{2,1,0:T(8,128)}, f32[2,384,768]{2,1,0:T(8,128)}, f32[2,384,768]{2,1,0:T(8,128)}, f32[2,384,768]{2,1,0:T(8,128)}) custom-call(s32[5]{0:T(128)} %stack.37.places_ref, bf16[1,2048,6144]{2,1,0:T(8,128)(2,1)} %bitcast.70, bf16[1,2048,1536]{2,1,0:T(8,128)(2,1)} %bitcast.76, f32[2,384,768]{2,1,0:T(8,128)} %collective-permute-done.33.refs_0_, ...), custom_call_target="tpu_custom_call" | custom-call | flops 9663676416 | bytes 18874368 | tf_op jit(solution)/shard_map/pallas_call | solution.py:324
  1021.4 12.6 shard_map.147
  1034.0 35.8 %attn_bwd.7 = (bf16[4,4,512,1536]{3,2,1,0:T(8,128)(2,1)}, f32[2,512,1536]{2,1,0:T(8,128)}, f32[2,512,1536]{2,1,0:T(8,128)}) custom-call(bf16[512,1536]{1,0:T(8,128)(2,1)} %get-tuple-element.134.q_ref, bf16[512,3072]{1,0:T(8,128)(2,1)} %get-tuple-element.133.refs_3_.refs_5_.refs_7_.ko_ref.vo_ref, ...), custom_call_target="tpu_custom_call", output_to_operand_aliasing={{0}: (7, {})} | custom-call | flops 32212254720 | bytes 25165824 | tf_op jit(solution)/shard_map/attn_bwd/pallas_call | solution.py:206
  1077.9 7.1 fusion.7.acc0_hbm
  1085.0 14.7 d_kv.7
  1099.7 75.6 %all-to-all-done.1 = bf16[8,512,768]{2,1,0:T(8,128)(2,1)} async-done(((bf16[8,512,768]{2,1,0:T(8,128)(2,1)}), bf16[8,512,768]{2,1,0:T(8,128)(2,1)}, u32[]{:S(2)}, u32[]{:S(2)}) %all-to-all-start.1) | async-done | bytes 6291488 | tf_op jit(solution)/shard_map/all_to_all | solution.py:689
  1178.8 19.3 %shard_map.148 = (f32[2,384,768]{2,1,0:T(8,128)}, f32[2,384,768]{2,1,0:T(8,128)}, f32[2,384,768]{2,1,0:T(8,128)}, f32[2,384,768]{2,1,0:T(8,128)}) custom-call(s32[5]{0:T(128)} %stack.39.places_ref, bf16[4,2048,1536]{2,1,0:T(8,128)(2,1)} %bitcast.56, bf16[2,2048,1536]{2,1,0:T(8,128)(2,1)} %bitcast.62), custom_call_target="tpu_custom_call" | custom-call | flops 9663676416 | bytes 18874368 | tf_op jit(solution)/shard_map/pallas_call | solution.py:324
  1198.9 47.3 %collective-permute-done.59 = f32[2,384,768]{2,1,0:T(8,128)} collective-permute-done((f32[2,384,768]{2,1,0:T(8,128)}, f32[2,384,768]{2,1,0:T(8,128)}, u32[]{:S(2)}, u32[]{:S(2)}) %collective-permute-start.59) | collective-permute-done | bytes 2359328 | tf_op jit(solution)/shard_map/ppermute | solution.py:27
  1246.7 11.5 shard_map.149
  1274.9 21.3 %shard_map.150 = (f32[2,384,768]{2,1,0:T(8,128)}, f32[2,384,768]{2,1,0:T(8,128)}, f32[2,384,768]{2,1,0:T(8,128)}, f32[2,384,768]{2,1,0:T(8,128)}) custom-call(s32[5]{0:T(128)} %stack.37.places_ref, bf16[4,2048,1536]{2,1,0:T(8,128)(2,1)} %bitcast.58, bf16[2,2048,1536]{2,1,0:T(8,128)(2,1)} %bitcast.64, f32[2,384,768]{2,1,0:T(8,128)} %collective-permute-done.40.refs_0_, ...), custom_call_target="tpu_custom_call" | custom-call | flops 9663676416 | bytes 18874368 | tf_op jit(solution)/shard_map/pallas_call | solution.py:324
  1300.7 12.6 shard_map.151
  1318.6 16.5 fusion.24
  1335.0 11.9 shard_map.155
  1346.9 10.0 fusion.2
  1364.3 33.7 %collective-permute-done.71 = bf16[512,1536]{1,0:T(8,128)(2,1)} collective-permute-done((bf16[512,1536]{1,0:T(8,128)(2,1)}, bf16[512,1536]{1,0:T(8,128)(2,1)}, u32[]{:S(2)}, u32[]{:S(2)}) %collective-permute-start.71) | collective-permute-done | bytes 1572896 | tf_op jit(solution)/shard_map/ppermute | solution.py:740
  1398.0 10.0 fusion
  1408.4 11.5 shard_map.152
  1420.0 79.6 %all-to-all-done.3 = bf16[8,512,768]{2,1,0:T(8,128)(2,1)} async-done(((bf16[8,512,768]{2,1,0:T(8,128)(2,1)}), bf16[8,512,768]{2,1,0:T(8,128)(2,1)}, u32[]{:S(2)}, u32[]{:S(2)}) %all-to-all-start.3) | async-done | bytes 6291488 | tf_op jit(solution)/shard_map/all_to_all | solution.py:689
  1508.7 12.8 shard_map.156
  1530.5 16.3 fusion.25
  1546.8 10.2 collective-permute-done.60
  1566.2 22.0 %add_add_fusion.refs_0_ = f32[768,1536]{1,0:T(8,128)} fusion(f32[768,1536]{1,0:T(8,128)} %fusion.25, f32[768,1536]{1,0:T(8,128)} %fusion.24, f32[768,1536]{1,0:T(8,128)} %fusion.2, f32[768,1536]{1,0:T(8,128)} %fusion, bf16[4096,768]{1,0:T(8,128)(2,1)} %bitcast.27, bf16[4096,1536]{1,0:T(8,128)(2,1)} %all-gather.14.cloned.1.call-done), kind=kOutput, calls=%fused_computation.3 | convolution fusion | flops 9668395008 | bytes 42467328 | tf_op jit(solution)/shard_map/dot_general | solution.py:39
  1588.2 24.3 %collective-permute-done.48 = f32[2,384,768]{2,1,0:T(8,128)} collective-permute-done((f32[2,384,768]{2,1,0:T(8,128)}, f32[2,384,768]{2,1,0:T(8,128)}, u32[]{:S(2)}, u32[]{:S(2)}) %collective-permute-start.48) | collective-permute-done | bytes 2359328 | tf_op jit(solution)/shard_map/ppermute | solution.py:27
  1616.9 73.3 %collective-permute-done.50 = f32[2,384,768]{2,1,0:T(8,128)} collective-permute-done((f32[2,384,768]{2,1,0:T(8,128)}, f32[2,384,768]{2,1,0:T(8,128)}, u32[]{:S(2)}, u32[]{:S(2)}) %collective-permute-start.50) | collective-permute-done | bytes 2359328 | tf_op jit(solution)/shard_map/ppermute | solution.py:31
  1691.6 12.6 shard_map.153
  1717.8 9.6 collective-permute-done.70
  1735.4 8.7 shard_map.157
  1744.2 8.5 shard_map.154
  1752.7 10.2 shard_map.158
  (261 shorter events, 266.6 us)
Async XLA Ops:
  7.2 304.6 %all-gather.6.cloned.1.call-start = ((), (), s32[]{:S(2)}) async-start(), calls=%async_computation.4 | async-start | bytes 15925248 | tf_op jit(solution)/shard_map/all_gather | solution.py:647
  16.1 336.2 %all-gather.8.cloned.1.call-start = ((), (), s32[]{:S(2)}) async-start(), calls=%async_computation.5 | async-start | bytes 5308416 | tf_op jit(solution)/shard_map/all_gather | solution.py:647
  26.5 50.1 %collective-permute-start.2 = (bf16[384,1536]{1,0:T(8,128)(2,1)}, bf16[384,1536]{1,0:T(8,128)(2,1)}, u32[]{:S(2)}, u32[]{:S(2)}) collective-permute-start(bf16[384,1536]{1,0:T(8,128)(2,1)} %get-tuple-element.268), channel_id=1, source_target_pairs={{0,2},{2,0},{4,6},{6,4},{1,3},{3,1},{5,7},{7,5}} | collective-permute-start | bytes 3538952 | tf_op jit(solution)/shard_map/ppermute | solution.py:27
  29.9 145.5 %collective-permute-start.6 = (bf16[384,1536]{1,0:T(8,128)(2,1)}, bf16[384,1536]{1,0:T(8,128)(2,1)}, u32[]{:S(2)}, u32[]{:S(2)}) collective-permute-start(bf16[384,1536]{1,0:T(8,128)(2,1)} %get-tuple-element.268), channel_id=1, source_target_pairs={{0,4},{4,0},{2,6},{6,2},{1,5},{5,1},{3,7},{7,3}} | collective-permute-start | bytes 3538952 | tf_op jit(solution)/shard_map/ppermute | solution.py:31
  34.3 133.4 %collective-permute-start = (bf16[512,1536]{1,0:T(8,128)(2,1)}, bf16[512,1536]{1,0:T(8,128)(2,1)}, u32[]{:S(2)}, u32[]{:S(2)}) collective-permute-start(bf16[512,1536]{1,0:T(8,128)(2,1)} %dynamic-slice_bitcast_fusion.2), channel_id=1, source_target_pairs={{0,1},{1,0},{2,3},{3,2},{4,5},{5,4},{6,7},{7,6}} | collective-permute-start | bytes 4718600 | tf_op jit(solution)/shard_map/ppermute | solution.py:35
  34.8 92.4 %collective-permute-start.4 = (bf16[384,1536]{1,0:T(8,128)(2,1)}, bf16[384,1536]{1,0:T(8,128)(2,1)}, u32[]{:S(2)}, u32[]{:S(2)}) collective-permute-start(bf16[384,1536]{1,0:T(8,128)(2,1)} %get-tuple-element.267), channel_id=1, source_target_pairs={{0,2},{2,0},{4,6},{6,4},{1,3},{3,1},{5,7},{7,5}} | collective-permute-start | bytes 3538952 | tf_op jit(solution)/shard_map/ppermute | solution.py:27
  38.1 127.9 %collective-permute-start.14 = (bf16[384,1536]{1,0:T(8,128)(2,1)}, bf16[384,1536]{1,0:T(8,128)(2,1)}, u32[]{:S(2)}, u32[]{:S(2)}) collective-permute-start(bf16[384,1536]{1,0:T(8,128)(2,1)} %get-tuple-element.254), channel_id=1, source_target_pairs={{0,2},{2,0},{4,6},{6,4},{1,3},{3,1},{5,7},{7,5}} | collective-permute-start | bytes 3538952 | tf_op jit(solution)/shard_map/ppermute | solution.py:27
  40.5 1278.1 %all-gather.10.cloned.1.call-start = ((), (), s32[]{:S(2)}) async-start(), calls=%async_computation.6 | async-start | bytes 14155776 | tf_op jit(solution)/shard_map/all_gather | solution.py:647
  76.6 93.4 %collective-permute-start.3 = (bf16[384,1536]{1,0:T(8,128)(2,1)}, bf16[384,1536]{1,0:T(8,128)(2,1)S(1)}, u32[]{:S(2)}, u32[]{:S(2)}) collective-permute-start(bf16[384,1536]{1,0:T(8,128)(2,1)} %collective-permute-done.2), channel_id=1, source_target_pairs={{0,1},{1,0},{2,3},{3,2},{4,5},{5,4},{6,7},{7,6}} | collective-permute-start | bytes 3538952 | tf_op jit(solution)/shard_map/ppermute | solution.py:35
  127.2 78.0 %collective-permute-start.16 = (bf16[384,1536]{1,0:T(8,128)(2,1)S(1)}, bf16[384,1536]{1,0:T(8,128)(2,1)S(1)}, u32[]{:S(2)}, u32[]{:S(2)}) collective-permute-start(bf16[384,1536]{1,0:T(8,128)(2,1)S(1)} %get-tuple-element.253), channel_id=1, source_target_pairs={{0,2},{2,0},{4,6},{6,4},{1,3},{3,1},{5,7},{7,5}} | collective-permute-start | bytes 3538952 | tf_op jit(solution)/shard_map/ppermute | solution.py:27
  166.1 41.7 %collective-permute-start.18 = (bf16[384,1536]{1,0:T(8,128)(2,1)}, bf16[384,1536]{1,0:T(8,128)(2,1)S(1)}, u32[]{:S(2)}, u32[]{:S(2)}) collective-permute-start(bf16[384,1536]{1,0:T(8,128)(2,1)} %get-tuple-element.254), channel_id=1, source_target_pairs={{0,4},{4,0},{2,6},{6,2},{1,5},{5,1},{3,7},{7,3}} | collective-permute-start | bytes 3538952 | tf_op jit(solution)/shard_map/ppermute | solution.py:31
  167.7 41.7 %collective-permute-start.15 = (bf16[384,1536]{1,0:T(8,128)(2,1)}, bf16[384,1536]{1,0:T(8,128)(2,1)S(1)}, u32[]{:S(2)}, u32[]{:S(2)}) collective-permute-start(bf16[384,1536]{1,0:T(8,128)(2,1)} %collective-permute-done.14), channel_id=1, source_target_pairs={{0,1},{1,0},{2,3},{3,2},{4,5},{5,4},{6,7},{7,6}} | collective-permute-start | bytes 3538952 | tf_op jit(solution)/shard_map/ppermute | solution.py:35
  170.0 41.6 %collective-permute-start.5 = (bf16[384,1536]{1,0:T(8,128)(2,1)}, bf16[384,1536]{1,0:T(8,128)(2,1)S(1)}, u32[]{:S(2)}, u32[]{:S(2)}) collective-permute-start(bf16[384,1536]{1,0:T(8,128)(2,1)} %collective-permute-done.4), channel_id=1, source_target_pairs={{0,1},{1,0},{2,3},{3,2},{4,5},{5,4},{6,7},{7,6}} | collective-permute-start | bytes 3538952 | tf_op jit(solution)/shard_map/ppermute | solution.py:35
  175.3 57.7 %collective-permute-start.8 = (bf16[384,1536]{1,0:T(8,128)(2,1)}, bf16[384,1536]{1,0:T(8,128)(2,1)S(1)}, u32[]{:S(2)}, u32[]{:S(2)}) collective-permute-start(bf16[384,1536]{1,0:T(8,128)(2,1)} %get-tuple-element.267), channel_id=1, source_target_pairs={{0,4},{4,0},{2,6},{6,2},{1,5},{5,1},{3,7},{7,3}} | collective-permute-start | bytes 3538952 | tf_op jit(solution)/shard_map/ppermute | solution.py:31
  205.2 29.4 %collective-permute-start.17 = (bf16[384,1536]{1,0:T(8,128)(2,1)S(1)}, bf16[384,1536]{1,0:T(8,128)(2,1)S(1)}, u32[]{:S(2)}, u32[]{:S(2)}) collective-permute-start(bf16[384,1536]{1,0:T(8,128)(2,1)S(1)} %collective-permute-done.16), channel_id=1, source_target_pairs={{0,1},{1,0},{2,3},{3,2},{4,5},{5,4},{6,7},{7,6}} | collective-permute-start | bytes 3538952 | tf_op jit(solution)/shard_map/ppermute | solution.py:35
  207.8 50.5 %collective-permute-start.20 = (bf16[384,1536]{1,0:T(8,128)(2,1)S(1)}, bf16[384,1536]{1,0:T(8,128)(2,1)S(1)}, u32[]{:S(2)}, u32[]{:S(2)}) collective-permute-start(bf16[384,1536]{1,0:T(8,128)(2,1)S(1)} %get-tuple-element.253), channel_id=1, source_target_pairs={{0,4},{4,0},{2,6},{6,2},{1,5},{5,1},{3,7},{7,3}} | collective-permute-start | bytes 3538952 | tf_op jit(solution)/shard_map/ppermute | solution.py:31
  209.4 49.5 %collective-permute-start.7 = (bf16[384,1536]{1,0:T(8,128)(2,1)}, bf16[384,1536]{1,0:T(8,128)(2,1)S(1)}, u32[]{:S(2)}, u32[]{:S(2)}) collective-permute-start(bf16[384,1536]{1,0:T(8,128)(2,1)} %collective-permute-done.6), channel_id=1, source_target_pairs={{0,1},{1,0},{2,3},{3,2},{4,5},{5,4},{6,7},{7,6}} | collective-permute-start | bytes 3538952 | tf_op jit(solution)/shard_map/ppermute | solution.py:35
  211.6 52.2 %collective-permute-start.19 = (bf16[384,1536]{1,0:T(8,128)(2,1)S(1)}, bf16[384,1536]{1,0:T(8,128)(2,1)S(1)}, u32[]{:S(2)}, u32[]{:S(2)}) collective-permute-start(bf16[384,1536]{1,0:T(8,128)(2,1)S(1)} %collective-permute-done.18), channel_id=1, source_target_pairs={{0,1},{1,0},{2,3},{3,2},{4,5},{5,4},{6,7},{7,6}} | collective-permute-start | bytes 3538952 | tf_op jit(solution)/shard_map/ppermute | solution.py:35
  233.0 50.7 %collective-permute-start.10 = (bf16[384,1536]{1,0:T(8,128)(2,1)}, bf16[384,1536]{1,0:T(8,128)(2,1)}, u32[]{:S(2)}, u32[]{:S(2)}) collective-permute-start(bf16[384,1536]{1,0:T(8,128)(2,1)} %collective-permute-done.2), channel_id=1, source_target_pairs={{0,4},{4,0},{2,6},{6,2},{1,5},{5,1},{3,7},{7,3}} | collective-permute-start | bytes 3538952 | tf_op jit(solution)/shard_map/ppermute | solution.py:31
  234.6 31.4 %collective-permute-start.9 = (bf16[384,1536]{1,0:T(8,128)(2,1)S(1)}, bf16[384,1536]{1,0:T(8,128)(2,1)S(1)}, u32[]{:S(2)}, u32[]{:S(2)}) collective-permute-start(bf16[384,1536]{1,0:T(8,128)(2,1)S(1)} %collective-permute-done.8), channel_id=1, source_target_pairs={{0,1},{1,0},{2,3},{3,2},{4,5},{5,4},{6,7},{7,6}} | collective-permute-start | bytes 3538952 | tf_op jit(solution)/shard_map/ppermute | solution.py:35
  258.3 28.8 %collective-permute-start.12 = (bf16[384,1536]{1,0:T(8,128)(2,1)S(1)}, bf16[384,1536]{1,0:T(8,128)(2,1)S(1)}, u32[]{:S(2)}, u32[]{:S(2)}) collective-permute-start(bf16[384,1536]{1,0:T(8,128)(2,1)S(1)} %collective-permute-done.8), channel_id=1, source_target_pairs={{0,2},{2,0},{4,6},{6,4},{1,3},{3,1},{5,7},{7,5}} | collective-permute-start | bytes 3538952 | tf_op jit(solution)/shard_map/ppermute | solution.py:27
  258.9 49.5 %collective-permute-start.22 = (bf16[384,1536]{1,0:T(8,128)(2,1)}, bf16[384,1536]{1,0:T(8,128)(2,1)S(1)}, u32[]{:S(2)}, u32[]{:S(2)}) collective-permute-start(bf16[384,1536]{1,0:T(8,128)(2,1)} %collective-permute-done.14), channel_id=1, source_target_pairs={{0,4},{4,0},{2,6},{6,2},{1,5},{5,1},{3,7},{7,3}} | collective-permute-start | bytes 3538952 | tf_op jit(solution)/shard_map/ppermute | solution.py:31
  263.8 72.7 %collective-permute-start.21 = (bf16[384,1536]{1,0:T(8,128)(2,1)S(1)}, bf16[384,1536]{1,0:T(8,128)(2,1)}, u32[]{:S(2)}, u32[]{:S(2)}) collective-permute-start(bf16[384,1536]{1,0:T(8,128)(2,1)S(1)} %collective-permute-done.20), channel_id=1, source_target_pairs={{0,1},{1,0},{2,3},{3,2},{4,5},{5,4},{6,7},{7,6}} | collective-permute-start | bytes 3538952 | tf_op jit(solution)/shard_map/ppermute | solution.py:35
  266.0 74.6 %collective-permute-start.24 = (bf16[384,1536]{1,0:T(8,128)(2,1)S(1)}, bf16[384,1536]{1,0:T(8,128)(2,1)}, u32[]{:S(2)}, u32[]{:S(2)}) collective-permute-start(bf16[384,1536]{1,0:T(8,128)(2,1)S(1)} %collective-permute-done.20), channel_id=1, source_target_pairs={{0,2},{2,0},{4,6},{6,4},{1,3},{3,1},{5,7},{7,5}} | collective-permute-start | bytes 3538952 | tf_op jit(solution)/shard_map/ppermute | solution.py:27
  283.7 56.9 %collective-permute-start.11 = (bf16[384,1536]{1,0:T(8,128)(2,1)}, bf16[384,1536]{1,0:T(8,128)(2,1)}, u32[]{:S(2)}, u32[]{:S(2)}) collective-permute-start(bf16[384,1536]{1,0:T(8,128)(2,1)} %collective-permute-done.10), channel_id=1, source_target_pairs={{0,1},{1,0},{2,3},{3,2},{4,5},{5,4},{6,7},{7,6}} | collective-permute-start | bytes 3538952 | tf_op jit(solution)/shard_map/ppermute | solution.py:35
  287.1 61.7 %collective-permute-start.13 = (bf16[384,1536]{1,0:T(8,128)(2,1)S(1)}, bf16[384,1536]{1,0:T(8,128)(2,1)}, u32[]{:S(2)}, u32[]{:S(2)}) collective-permute-start(bf16[384,1536]{1,0:T(8,128)(2,1)S(1)} %collective-permute-done.12), channel_id=1, source_target_pairs={{0,1},{1,0},{2,3},{3,2},{4,5},{5,4},{6,7},{7,6}} | collective-permute-start | bytes 3538952 | tf_op jit(solution)/shard_map/ppermute | solution.py:35
  308.3 35.8 %collective-permute-start.23 = (bf16[384,1536]{1,0:T(8,128)(2,1)S(1)}, bf16[384,1536]{1,0:T(8,128)(2,1)}, u32[]{:S(2)}, u32[]{:S(2)}) collective-permute-start(bf16[384,1536]{1,0:T(8,128)(2,1)S(1)} %collective-permute-done.22), channel_id=1, source_target_pairs={{0,1},{1,0},{2,3},{3,2},{4,5},{5,4},{6,7},{7,6}} | collective-permute-start | bytes 3538952 | tf_op jit(solution)/shard_map/ppermute | solution.py:35
  735.1 795.4 %all-gather.12.cloned.1.call-start = ((), (), s32[]{:S(2)}) async-start(), calls=%async_computation.7 | async-start | bytes 14155776 | tf_op jit(solution)/shard_map/all_gather | solution.py:647
  994.0 26.0 %collective-permute-start.37 = (f32[2,384,768]{2,1,0:T(8,128)}, f32[2,384,768]{2,1,0:T(8,128)S(1)}, u32[]{:S(2)}, u32[]{:S(2)}) collective-permute-start(f32[2,384,768]{2,1,0:T(8,128)} %get-tuple-element.196), channel_id=1, source_target_pairs={{0,1},{1,0},{2,3},{3,2},{4,5},{5,4},{6,7},{7,6}} | collective-permute-start | bytes 7077896 | tf_op jit(solution)/shard_map/ppermute | solution.py:35
  994.2 25.9 %collective-permute-start.38 = (f32[2,384,768]{2,1,0:T(8,128)}, f32[2,384,768]{2,1,0:T(8,128)}, u32[]{:S(2)}, u32[]{:S(2)}) collective-permute-start(f32[2,384,768]{2,1,0:T(8,128)} %get-tuple-element.197), channel_id=1, source_target_pairs={{0,1},{1,0},{2,3},{3,2},{4,5},{5,4},{6,7},{7,6}} | collective-permute-start | bytes 7077896 | tf_op jit(solution)/shard_map/ppermute | solution.py:35
  995.1 75.2 %all-to-all-start.2 = ((bf16[8,512,768]{2,1,0:T(8,128)(2,1)}), bf16[8,512,768]{2,1,0:T(8,128)(2,1)}, u32[]{:S(2)}, u32[]{:S(2)}) async-start(bf16[8,512,768]{2,1,0:T(8,128)(2,1)} %get-tuple-element.248), calls=%async_computation.2 | async-start | bytes 12582912 | tf_op jit(solution)/shard_map/all_to_all | solution.py:689
  1070.4 104.9 %all-to-all-start.1 = ((bf16[8,512,768]{2,1,0:T(8,128)(2,1)}), bf16[8,512,768]{2,1,0:T(8,128)(2,1)}, u32[]{:S(2)}, u32[]{:S(2)}) async-start(bf16[8,512,768]{2,1,0:T(8,128)(2,1)} %get-tuple-element.246), calls=%async_computation.1 | async-start | bytes 12582912 | tf_op jit(solution)/shard_map/all_to_all | solution.py:689
  1073.9 492.3 %all-gather.14.cloned.1.call-start = ((), (), s32[]{:S(2)}) async-start(), calls=%async_computation.8 | async-start | bytes 14155776 | tf_op jit(solution)/shard_map/all_gather | solution.py:647
  1074.5 171.7 %collective-permute-start.59 = (f32[2,384,768]{2,1,0:T(8,128)}, f32[2,384,768]{2,1,0:T(8,128)}, u32[]{:S(2)}, u32[]{:S(2)}) collective-permute-start(f32[2,384,768]{2,1,0:T(8,128)} %get-tuple-element.199), channel_id=1, source_target_pairs={{0,2},{2,0},{4,6},{6,4},{1,3},{3,1},{5,7},{7,5}} | collective-permute-start | bytes 7077896 | tf_op jit(solution)/shard_map/ppermute | solution.py:27
  1076.4 169.8 %collective-permute-start.62 = (f32[2,384,768]{2,1,0:T(8,128)}, f32[2,384,768]{2,1,0:T(8,128)}, u32[]{:S(2)}, u32[]{:S(2)}) collective-permute-start(f32[2,384,768]{2,1,0:T(8,128)} %get-tuple-element.200), channel_id=1, source_target_pairs={{0,4},{4,0},{2,6},{6,2},{1,5},{5,1},{3,7},{7,3}} | collective-permute-start | bytes 7077896 | tf_op jit(solution)/shard_map/ppermute | solution.py:31
  1175.3 139.3 %all-to-all-start = ((bf16[8,512,768]{2,1,0:T(8,128)(2,1)}), bf16[8,512,768]{2,1,0:T(8,128)(2,1)}, u32[]{:S(2)}, u32[]{:S(2)}) async-start(bf16[8,512,768]{2,1,0:T(8,128)(2,1)} %get-tuple-element.244), calls=%async_computation | async-start | bytes 12582912 | tf_op jit(solution)/shard_map/all_to_all | solution.py:689
  1198.1 60.1 %collective-permute-start.40 = (f32[2,384,768]{2,1,0:T(8,128)}, f32[2,384,768]{2,1,0:T(8,128)}, u32[]{:S(2)}, u32[]{:S(2)}) collective-permute-start(f32[2,384,768]{2,1,0:T(8,128)} %get-tuple-element.214), channel_id=1, source_target_pairs={{0,1},{1,0},{2,3},{3,2},{4,5},{5,4},{6,7},{7,6}} | collective-permute-start | bytes 7077896 | tf_op jit(solution)/shard_map/ppermute | solution.py:35
  1198.4 59.9 %collective-permute-start.68 = (bf16[512,1536]{1,0:T(8,128)(2,1)}, bf16[512,1536]{1,0:T(8,128)(2,1)}, u32[]{:S(2)}, u32[]{:S(2)}) collective-permute-start(bf16[512,1536]{1,0:T(8,128)(2,1)} %get-tuple-element.252), channel_id=1, source_target_pairs={{0,1},{1,0},{2,3},{3,2},{4,5},{5,4},{6,7},{7,6}} | collective-permute-start | bytes 4718600 | tf_op jit(solution)/shard_map/ppermute | solution.py:35
  1198.6 67.7 %collective-permute-start.41 = (f32[2,384,768]{2,1,0:T(8,128)}, f32[2,384,768]{2,1,0:T(8,128)S(1)}, u32[]{:S(2)}, u32[]{:S(2)}) collective-permute-start(f32[2,384,768]{2,1,0:T(8,128)} %get-tuple-element.215), channel_id=1, source_target_pairs={{0,1},{1,0},{2,3},{3,2},{4,5},{5,4},{6,7},{7,6}} | collective-permute-start | bytes 7077896 | tf_op jit(solution)/shard_map/ppermute | solution.py:35
  1246.2 24.8 %collective-permute-start.42 = (f32[2,384,768]{2,1,0:T(8,128)}, f32[2,384,768]{2,1,0:T(8,128)}, u32[]{:S(2)}, u32[]{:S(2)}) collective-permute-start(f32[2,384,768]{2,1,0:T(8,128)} %get-tuple-element.216), channel_id=1, source_target_pairs={{0,1},{1,0},{2,3},{3,2},{4,5},{5,4},{6,7},{7,6}} | collective-permute-start | bytes 7077896 | tf_op jit(solution)/shard_map/ppermute | solution.py:35
  1246.2 26.2 %collective-permute-start.43 = (f32[2,384,768]{2,1,0:T(8,128)}, f32[2,384,768]{2,1,0:T(8,128)}, u32[]{:S(2)}, u32[]{:S(2)}) collective-permute-start(f32[2,384,768]{2,1,0:T(8,128)} %get-tuple-element.217), channel_id=1, source_target_pairs={{0,1},{1,0},{2,3},{3,2},{4,5},{5,4},{6,7},{7,6}} | collective-permute-start | bytes 7077896 | tf_op jit(solution)/shard_map/ppermute | solution.py:35
  1258.2 38.0 %collective-permute-start.44 = (f32[2,384,768]{2,1,0:T(8,128)}, f32[2,384,768]{2,1,0:T(8,128)}, u32[]{:S(2)}, u32[]{:S(2)}) collective-permute-start(f32[2,384,768]{2,1,0:T(8,128)} %get-tuple-element.219), channel_id=1, source_target_pairs={{0,1},{1,0},{2,3},{3,2},{4,5},{5,4},{6,7},{7,6}} | collective-permute-start | bytes 7077896 | tf_op jit(solution)/shard_map/ppermute | solution.py:35
  1258.3 41.0 %collective-permute-start.45 = (f32[2,384,768]{2,1,0:T(8,128)}, f32[2,384,768]{2,1,0:T(8,128)}, u32[]{:S(2)}, u32[]{:S(2)}) collective-permute-start(f32[2,384,768]{2,1,0:T(8,128)} %get-tuple-element.220), channel_id=1, source_target_pairs={{0,1},{1,0},{2,3},{3,2},{4,5},{5,4},{6,7},{7,6}} | collective-permute-start | bytes 7077896 | tf_op jit(solution)/shard_map/ppermute | solution.py:35
  1267.7 89.1 %collective-permute-start.66 = (bf16[2048,1536]{1,0:T(8,128)(2,1)}, bf16[2048,1536]{1,0:T(8,128)(2,1)}, u32[]{:S(2)}, u32[]{:S(2)}) collective-permute-start(bf16[2048,1536]{1,0:T(8,128)(2,1)} %bitcast.89), channel_id=1, source_target_pairs={{0,1},{1,0},{2,3},{3,2},{4,5},{5,4},{6,7},{7,6}} | collective-permute-start | bytes 18874376 | tf_op jit(solution)/shard_map/ppermute | solution.py:35
  1271.0 93.3 %collective-permute-start.58 = (f32[2,384,768]{2,1,0:T(8,128)}, f32[2,384,768]{2,1,0:T(8,128)}, u32[]{:S(2)}, u32[]{:S(2)}) collective-permute-start(f32[2,384,768]{2,1,0:T(8,128)} %get-tuple-element.201), channel_id=1, source_target_pairs={{0,2},{2,0},{4,6},{6,4},{1,3},{3,1},{5,7},{7,5}} | collective-permute-start | bytes 7077896 | tf_op jit(solution)/shard_map/ppermute | solution.py:27
  1272.4 125.6 %collective-permute-start.71 = (bf16[512,1536]{1,0:T(8,128)(2,1)}, bf16[512,1536]{1,0:T(8,128)(2,1)}, u32[]{:S(2)}, u32[]{:S(2)}) collective-permute-start(bf16[512,1536]{1,0:T(8,128)(2,1)} %get-tuple-element.264), channel_id=1, source_target_pairs={{0,2},{2,0},{5,7},{7,5}} | collective-permute-start | bytes 4718600 | tf_op jit(solution)/shard_map/ppermute | solution.py:740
  1296.3 111.7 %collective-permute-start.69 = (bf16[512,1536]{1,0:T(8,128)(2,1)S(1)}, bf16[512,1536]{1,0:T(8,128)(2,1)}, u32[]{:S(2)}, u32[]{:S(2)}) collective-permute-start(bf16[512,1536]{1,0:T(8,128)(2,1)S(1)} %get-tuple-element.263), channel_id=1, source_target_pairs={{0,4},{2,6},{5,1},{7,3}} | collective-permute-start | bytes 4718600 | tf_op jit(solution)/shard_map/ppermute | solution.py:739
  1299.3 206.3 %collective-permute-start.49 = (f32[2,384,768]{2,1,0:T(8,128)}, f32[2,384,768]{2,1,0:T(8,128)}, u32[]{:S(2)}, u32[]{:S(2)}) collective-permute-start(f32[2,384,768]{2,1,0:T(8,128)} %get-tuple-element.222), channel_id=1, source_target_pairs={{0,2},{2,0},{4,6},{6,4},{1,3},{3,1},{5,7},{7,5}} | collective-permute-start | bytes 7077896 | tf_op jit(solution)/shard_map/ppermute | solution.py:27
  1314.7 184.9 %all-to-all-start.3 = ((bf16[8,512,768]{2,1,0:T(8,128)(2,1)}), bf16[8,512,768]{2,1,0:T(8,128)(2,1)}, u32[]{:S(2)}, u32[]{:S(2)}) async-start(bf16[8,512,768]{2,1,0:T(8,128)(2,1)} %get-tuple-element.250), calls=%async_computation.3 | async-start | bytes 12582912 | tf_op jit(solution)/shard_map/all_to_all | solution.py:689
  1356.9 150.6 %collective-permute-start.52 = (f32[2,384,768]{2,1,0:T(8,128)}, f32[2,384,768]{2,1,0:T(8,128)}, u32[]{:S(2)}, u32[]{:S(2)}) collective-permute-start(f32[2,384,768]{2,1,0:T(8,128)} %get-tuple-element.223), channel_id=1, source_target_pairs={{0,4},{4,0},{2,6},{6,2},{1,5},{5,1},{3,7},{7,3}} | collective-permute-start | bytes 7077896 | tf_op jit(solution)/shard_map/ppermute | solution.py:31
  1364.3 143.9 %collective-permute-start.56 = (f32[2,384,768]{2,1,0:T(8,128)}, f32[2,384,768]{2,1,0:T(8,128)}, u32[]{:S(2)}, u32[]{:S(2)}) collective-permute-start(f32[2,384,768]{2,1,0:T(8,128)} %get-tuple-element.239), channel_id=1, source_target_pairs={{0,1},{1,0},{2,3},{3,2},{4,5},{5,4},{6,7},{7,6}} | collective-permute-start | bytes 7077896 | tf_op jit(solution)/shard_map/ppermute | solution.py:35
  1398.0 110.2 %collective-permute-start.57 = (f32[2,384,768]{2,1,0:T(8,128)}, f32[2,384,768]{2,1,0:T(8,128)}, u32[]{:S(2)}, u32[]{:S(2)}) collective-permute-start(f32[2,384,768]{2,1,0:T(8,128)} %get-tuple-element.240), channel_id=1, source_target_pairs={{0,1},{1,0},{2,3},{3,2},{4,5},{5,4},{6,7},{7,6}} | collective-permute-start | bytes 7077896 | tf_op jit(solution)/shard_map/ppermute | solution.py:35
  1408.0 121.1 %collective-permute-start.61 = (f32[2,384,768]{2,1,0:T(8,128)}, f32[2,384,768]{2,1,0:T(8,128)}, u32[]{:S(2)}, u32[]{:S(2)}) collective-permute-start(f32[2,384,768]{2,1,0:T(8,128)} %get-tuple-element.205), channel_id=1, source_target_pairs={{0,4},{4,0},{2,6},{6,2},{1,5},{5,1},{3,7},{7,3}} | collective-permute-start | bytes 7077896 | tf_op jit(solution)/shard_map/ppermute | solution.py:31
  1505.5 51.4 %collective-permute-start.60 = (f32[2,384,768]{2,1,0:T(8,128)}, f32[2,384,768]{2,1,0:T(8,128)}, u32[]{:S(2)}, u32[]{:S(2)}) collective-permute-start(f32[2,384,768]{2,1,0:T(8,128)} %add.267), channel_id=1, source_target_pairs={{0,4},{4,0},{2,6},{6,2},{1,5},{5,1},{3,7},{7,3}} | collective-permute-start | bytes 7077896 | tf_op jit(solution)/shard_map/ppermute | solution.py:31
  1507.5 54.4 %collective-permute-start.63 = (f32[2,384,768]{2,1,0:T(8,128)}, f32[2,384,768]{2,1,0:T(8,128)}, u32[]{:S(2)}, u32[]{:S(2)}) collective-permute-start(f32[2,384,768]{2,1,0:T(8,128)} %add.270), channel_id=1, source_target_pairs={{0,2},{2,0},{4,6},{6,4},{1,3},{3,1},{5,7},{7,5}} | collective-permute-start | bytes 7077896 | tf_op jit(solution)/shard_map/ppermute | solution.py:27
  1508.2 57.4 %collective-permute-start.46 = (f32[2,384,768]{2,1,0:T(8,128)}, f32[2,384,768]{2,1,0:T(8,128)}, u32[]{:S(2)}, u32[]{:S(2)}) collective-permute-start(f32[2,384,768]{2,1,0:T(8,128)} %get-tuple-element.230), channel_id=1, source_target_pairs={{0,1},{1,0},{2,3},{3,2},{4,5},{5,4},{6,7},{7,6}} | collective-permute-start | bytes 7077896 | tf_op jit(solution)/shard_map/ppermute | solution.py:35
  1508.2 57.4 %collective-permute-start.47 = (f32[2,384,768]{2,1,0:T(8,128)}, f32[2,384,768]{2,1,0:T(8,128)}, u32[]{:S(2)}, u32[]{:S(2)}) collective-permute-start(f32[2,384,768]{2,1,0:T(8,128)} %get-tuple-element.231), channel_id=1, source_target_pairs={{0,1},{1,0},{2,3},{3,2},{4,5},{5,4},{6,7},{7,6}} | collective-permute-start | bytes 7077896 | tf_op jit(solution)/shard_map/ppermute | solution.py:35
  1529.1 83.4 %collective-permute-start.48 = (f32[2,384,768]{2,1,0:T(8,128)}, f32[2,384,768]{2,1,0:T(8,128)}, u32[]{:S(2)}, u32[]{:S(2)}) collective-permute-start(f32[2,384,768]{2,1,0:T(8,128)} %get-tuple-element.224), channel_id=1, source_target_pairs={{0,2},{2,0},{4,6},{6,4},{1,3},{3,1},{5,7},{7,5}} | collective-permute-start | bytes 7077896 | tf_op jit(solution)/shard_map/ppermute | solution.py:27
  1557.0 156.1 %collective-permute-start.51 = (f32[2,384,768]{2,1,0:T(8,128)}, f32[2,384,768]{2,1,0:T(8,128)}, u32[]{:S(2)}, u32[]{:S(2)}) collective-permute-start(f32[2,384,768]{2,1,0:T(8,128)} %get-tuple-element.228), channel_id=1, source_target_pairs={{0,4},{4,0},{2,6},{6,2},{1,5},{5,1},{3,7},{7,3}} | collective-permute-start | bytes 7077896 | tf_op jit(solution)/shard_map/ppermute | solution.py:31
  1561.9 165.4 %collective-permute-start.72 = (bf16[1024,1536]{1,0:T(8,128)(2,1)}, bf16[1024,1536]{1,0:T(8,128)(2,1)}, u32[]{:S(2)}, u32[]{:S(2)}) collective-permute-start(bf16[1024,1536]{1,0:T(8,128)(2,1)} %pad_maximum_fusion.2), channel_id=1, source_target_pairs={{0,4},{2,6},{5,1},{7,3}} | collective-permute-start | bytes 9437192 | tf_op jit(solution)/shard_map/ppermute | solution.py:744
  1565.6 124.6 %collective-permute-start.50 = (f32[2,384,768]{2,1,0:T(8,128)}, f32[2,384,768]{2,1,0:T(8,128)}, u32[]{:S(2)}, u32[]{:S(2)}) collective-permute-start(f32[2,384,768]{2,1,0:T(8,128)} %add.261), channel_id=1, source_target_pairs={{0,4},{4,0},{2,6},{6,2},{1,5},{5,1},{3,7},{7,3}} | collective-permute-start | bytes 7077896 | tf_op jit(solution)/shard_map/ppermute | solution.py:31
  1565.6 147.7 %collective-permute-start.53 = (f32[2,384,768]{2,1,0:T(8,128)}, f32[2,384,768]{2,1,0:T(8,128)}, u32[]{:S(2)}, u32[]{:S(2)}) collective-permute-start(f32[2,384,768]{2,1,0:T(8,128)} %add.264), channel_id=1, source_target_pairs={{0,2},{2,0},{4,6},{6,4},{1,3},{3,1},{5,7},{7,5}} | collective-permute-start | bytes 7077896 | tf_op jit(solution)/shard_map/ppermute | solution.py:27
  1612.5 140.2 %collective-permute-start.67 = (f32[768,1536]{1,0:T(8,128)}, f32[768,1536]{1,0:T(8,128)}, u32[]{:S(2)}, u32[]{:S(2)}) collective-permute-start(f32[768,1536]{1,0:T(8,128)} %add_add_fusion.refs_0_), channel_id=1, source_target_pairs={{0,1},{1,0},{2,3},{3,2},{4,5},{5,4},{6,7},{7,6}} | collective-permute-start | bytes 14155784 | tf_op jit(solution)/shard_map/ppermute | solution.py:35
  1690.2 37.2 %collective-permute-start.70 = (bf16[512,1536]{1,0:T(8,128)(2,1)}, bf16[512,1536]{1,0:T(8,128)(2,1)}, u32[]{:S(2)}, u32[]{:S(2)}) collective-permute-start(bf16[512,1536]{1,0:T(8,128)(2,1)} %broadcast_select_fusion.3), channel_id=1, source_target_pairs={{0,2},{2,0},{4,6},{6,4},{1,3},{3,1},{5,7},{7,5}} | collective-permute-start | bytes 4718600 | tf_op jit(solution)/shard_map/ppermute | solution.py:27
  (39 other events, 497.4 us)
Sparse Core Ops, SparseCore 0:
  16.2 129.8 all-gather.5
  148.4 52.1 all-gather.7
  735.2 66.2 all-gather.9
  831.4 65.9 all-gather.11
  1076.2 155.6 all-gather.13
